TPU v7x, 32 devices: a whole 2x2x4 slice. The times are simulated.
32 devices in a mesh: seq: 8 (over z, x), head: 4 (over y, core).
Axes of the slice: x: 2, y: 2, z: 4, core: 2. Of those that a mesh axis runs over, the one named last changes fastest.
Arguments:
- queries: bfloat16 [8192, 4096], P(('seq', 'head')), may hold values from -6 to 6
- keys: bfloat16 [8192, 4096], P(('seq', 'head')), may hold values from -6 to 6
- values: bfloat16 [8192, 4096], P(('seq', 'head')), may hold values from -6 to 6
- spikes: int32 [8192, 4096], P(('seq', 'head')), may hold values from 0 to 26
- gain: float32 [4096], P('head'), may hold values from 0.1 to 1.9
Outputs:
- attended: bfloat16 [8192, 4096], P('seq', 'head')
- cache: float32 [8, 32, 128, 128], P('seq', 'head')
Inputs may be any that keep to these rules, and one draw needn't show every extreme that they name: spikes codes count_query + 3 count_key + 9 count_value with each count 0, 1 or 2.
All inputs are finite; a program needn't handle non-finite values.
Results may differ from a plain program's by a relative error of at most 0.0027.
Values may be sent and summed in bfloat16 or wider, within the bound.
No kernel may reach another device: no remote copies, remote signals or barrier semaphores. Data moves between devices by JAX's collectives and lax.ppermute only.
A program may use at most 128 MiB of HBM per device.

v0:
```python
import jax
import jax.numpy as jnp
from jax import lax
from jax.sharding import PartitionSpec as P

HD = 128


def decode_counts(spikes):
    return (spikes % 3, spikes // 3 % 3, spikes // 9)


def per_device(queries, keys, values, spikes, gain):
    count_query, count_key, count_value = decode_counts(spikes)
    spiked_query = queries * count_query.astype(jnp.bfloat16)
    spiked_key = keys * count_key.astype(jnp.bfloat16)
    spiked_value = values * count_value.astype(jnp.bfloat16)
    query_block, key_block, value_block = (
        lax.all_to_all(spiked_query, "head", split_axis=1, concat_axis=0, tiled=True),
        lax.all_to_all(spiked_key, "head", split_axis=1, concat_axis=0, tiled=True),
        lax.all_to_all(spiked_value, "head", split_axis=1, concat_axis=0, tiled=True),
    )
    block_rows = key_block.shape[0]
    head_count = key_block.shape[1] // HD
    key_heads = key_block.reshape(block_rows, head_count, HD)
    value_heads = value_block.reshape(block_rows, head_count, HD)
    states = jnp.einsum("shd,she->hde", key_heads, value_heads, preferred_element_type=jnp.float32)
    block_index = lax.axis_index("seq")
    piece = lax.all_gather(states[None], "seq", axis=0, tiled=True)
    anchors = jnp.arange(piece.shape[0], dtype=jnp.int32)
    before = (anchors < block_index)[:, None, None, None]
    earlier_state = jnp.sum(jnp.where(before, piece, 0.0), axis=0)
    inclusive = earlier_state + states
    seen_tokens = ((block_index + 1) * block_rows).astype(jnp.float32)
    cache = (inclusive * lax.rsqrt(seen_tokens))[None]
    query_heads = query_block.reshape(block_rows, head_count, HD)
    score_scale = HD ** (-0.5)
    tile_rows = min(1024, block_rows)
    tile_count = block_rows // tile_rows
    causal = lax.broadcasted_iota(jnp.int32, (tile_rows, tile_rows), 0) >= lax.broadcasted_iota(
        jnp.int32, (tile_rows, tile_rows), 1
    )
    results = []
    for row_tile in range(tile_count):
        query_tile = query_heads[row_tile * tile_rows : (row_tile + 1) * tile_rows]
        total = (
            jnp.einsum(
                "thd,hde->the",
                query_tile.astype(jnp.float32),
                earlier_state,
                precision=lax.Precision.HIGHEST,
            )
            * score_scale
        )
        for col_tile in range(row_tile + 1):
            key_tile = key_heads[col_tile * tile_rows : (col_tile + 1) * tile_rows]
            value_tile = value_heads[col_tile * tile_rows : (col_tile + 1) * tile_rows]
            scores = (
                jnp.einsum("thd,shd->hts", query_tile, key_tile, preferred_element_type=jnp.float32)
                * score_scale
            )
            if col_tile == row_tile:
                scores = jnp.where(causal[None], scores, 0.0)
            weights = scores.astype(jnp.bfloat16)
            total = total + jnp.einsum(
                "hts,shd->thd", weights, value_tile, preferred_element_type=jnp.float32
            )
        results.append(total)
    raw = jnp.concatenate(results, axis=0)
    head_gain = gain.reshape(head_count, HD)
    normed = raw * lax.rsqrt(jnp.mean(raw * raw, axis=-1, keepdims=True) + 1e-06) * head_gain
    return (normed.reshape(block_rows, head_count * HD).astype(jnp.bfloat16), cache)


def solution(mesh):
    in_specs = (
        P(("seq", "head"), None),
        P(("seq", "head"), None),
        P(("seq", "head"), None),
        P(("seq", "head"), None),
        P("head"),
    )
    out_specs = (P("seq", "head"), P("seq", "head", None, None))
    return jax.shard_map(
        per_device, mesh=mesh, in_specs=in_specs, out_specs=out_specs, check_vma=False
    )
```

profile of v0, /device:TPU:0, one launch (start us, length us, event | category | flops | bytes accessed | tf_op | source)
XLA Modules:
  0.0 186.2 jit_solution(14525818200085226969)
XLA Ops:
  7.2 12.5 %fusion.14 = (bf16[256,4096]{1,0:T(8,128)(2,1)}, bf16[256,4096]{1,0:T(8,128)(2,1)S(1)}, bf16[256,4096]{1,0:T(8,128)(2,1)}) fusion(bf16[256,4096]{1,0:T(8,128)(2,1)} %param.5, s32[256,4096]{1,0:T(8,128)} %param.8, bf16[256,4096]{1,0:T(8,128)(2,1)} %param.7, bf16[256,4096]{1,0:T(8,128)(2,1)} %param.6), kind=kLoop, calls=%fused_computation.26 | loop fusion | flops 40894464 | bytes 16777216 | tf_op jit(solution)/shard_map/mul | solution.py:15
  19.6 1.5 copy.46
  21.1 4.2 %all-to-all-start.1 = ((bf16[256,4,1024]{2,0,1:T(8,128)(2,1)}), bf16[256,4,1024]{2,0,1:T(8,128)(2,1)S(1)}, u32[]{:S(2)}, u32[]{:S(2)}) async-start(bf16[256,4,1024]{2,0,1:T(8,128)(2,1)} %bitcast.42), calls=%async_computation.1 | async-start | bytes 4194304 | tf_op jit(solution)/shard_map/all_to_all | solution.py:21
  25.4 4.1 %copy.19 = bf16[256,4096]{0,1:T(8,128)(2,1)} copy(bf16[256,4096]{1,0:T(8,128)(2,1)} %get-tuple-element.10) | data formatting | bytes 4194304 | tf_op jit(solution)/shard_map/mul | solution.py:16
  29.4 21.6 %all-to-all-done.1 = bf16[256,4,1024]{2,0,1:T(8,128)(2,1)S(1)} async-done(((bf16[256,4,1024]{2,0,1:T(8,128)(2,1)}), bf16[256,4,1024]{2,0,1:T(8,128)(2,1)S(1)}, u32[]{:S(2)}, u32[]{:S(2)}) %all-to-all-start.1) | async-done | bytes 2097184 | tf_op jit(solution)/shard_map/all_to_all | solution.py:21
  51.1 4.5 %all-to-all-start = ((bf16[256,4,1024]{0,2,1:T(8,128)(2,1)}), bf16[256,4,1024]{0,2,1:T(8,128)(2,1)}, u32[]{:S(2)}, u32[]{:S(2)}) async-start(bf16[256,4,1024]{0,2,1:T(8,128)(2,1)} %bitcast.41), calls=%async_computation | async-start | bytes 4194304 | tf_op jit(solution)/shard_map/all_to_all | solution.py:20
  55.5 0.0 all-gather.3.cloned.1.call-start
  55.6 1.9 %copy.34 = bf16[128,8,8,128]{3,2,1,0:T(8,128)(2,1)} copy(bf16[128,8,8,128]{3,1,2,0:T(8,128)(2,1)S(1)} %bitcast.40) | data formatting | bytes 4194304
  57.5 3.2 %copy.28 = bf16[1024,8,128]{0,2,1:T(8,128)(2,1)S(1)} copy(bf16[1024,8,128]{2,1,0:T(8,128)(2,1)} %bitcast.43) | data formatting | bytes 4194304 | tf_op jit(solution)/shard_map/reshape | solution.py:26
  60.8 20.5 %all-to-all-done = bf16[256,4,1024]{0,2,1:T(8,128)(2,1)} async-done(((bf16[256,4,1024]{0,2,1:T(8,128)(2,1)}), bf16[256,4,1024]{0,2,1:T(8,128)(2,1)}, u32[]{:S(2)}, u32[]{:S(2)}) %all-to-all-start) | async-done | bytes 2097184 | tf_op jit(solution)/shard_map/all_to_all | solution.py:20
  81.3 4.6 %copy.20 = bf16[4,256,1024]{1,0,2:T(4,128)(2,1)} copy(bf16[4,256,1024]{1,2,0:T(8,128)(2,1)} %bitcast.1) | data formatting | bytes 4194304 | tf_op jit(solution)/shard_map/all_to_all | solution.py:20
  85.9 4.5 %reshape.47 = bf16[1024,8,128]{0,2,1:T(8,128)(2,1)} reshape(bf16[4,256,1024]{1,0,2:T(4,128)(2,1)} %copy.20) | data formatting | bytes 4194304 | tf_op jit(solution)/shard_map/reshape | solution.py:25
  90.3 3.1 %fusion.22 = f32[8,128,128]{2,1,0:T(8,128)} fusion(bf16[1024,8,128]{0,2,1:T(8,128)(2,1)} %reshape.47, bf16[1024,8,128]{0,2,1:T(8,128)(2,1)S(1)} %copy.28), kind=kOutput, calls=%fused_computation.38 | convolution fusion | flops 268435456 | bytes 4718592 | tf_op jit(solution)/shard_map/shd,she->hde/dot_general | solution.py:27
  93.4 0.0 all-gather.3.cloned.1.call-update
  93.4 3.2 %copy.45 = bf16[32,4,8,1024]{3,2,0,1:T(8,128)(2,1)} copy(bf16[32,4,8,1024]{3,2,1,0:T(8,128)(2,1)} %bitcast.47) | data formatting | bytes 4194304 | tf_op jit(solution)/shard_map/all_to_all | solution.py:19
  96.6 4.6 %all-to-all-start.2 = ((bf16[256,4,1024]{2,0,1:T(8,128)(2,1)}), bf16[256,4,1024]{2,0,1:T(8,128)(2,1)}, u32[]{:S(2)}, u32[]{:S(2)}) async-start(bf16[256,4,1024]{2,0,1:T(8,128)(2,1)} %bitcast.39), calls=%async_computation.2 | async-start | bytes 4194304 | tf_op jit(solution)/shard_map/all_to_all | solution.py:19
  101.3 0.3 iota_compare_fusion
  101.6 25.2 %all-to-all-done.2 = bf16[256,4,1024]{2,0,1:T(8,128)(2,1)} async-done(((bf16[256,4,1024]{2,0,1:T(8,128)(2,1)}), bf16[256,4,1024]{2,0,1:T(8,128)(2,1)}, u32[]{:S(2)}, u32[]{:S(2)}) %all-to-all-start.2) | async-done | bytes 2097184 | tf_op jit(solution)/shard_map/all_to_all | solution.py:19
  126.8 3.5 %copy.35 = bf16[128,8,8,128]{3,2,1,0:T(8,128)(2,1)} copy(bf16[128,8,8,128]{3,1,2,0:T(8,128)(2,1)} %bitcast.18) | data formatting | bytes 4194304
  130.4 13.3 %fusion = f32[8,128,1024]{2,1,0:T(8,128)} fusion(bf16[1024,8,128]{0,2,1:T(8,128)(2,1)S(1)} %copy.28, pred[1024,1024]{1,0:T(8,128)(4,1)S(1)} %iota_compare_fusion, bf16[1024,8,128]{0,2,1:T(8,128)(2,1)} %reshape.47, bf16[1024,8,128]{2,1,0:T(8,128)(2,1)} %bitcast.44), kind=kOutput, calls=%fused_computation.1 | convolution fusion | flops 4320133120 | bytes 11534336 | tf_op jit(solution)/shard_map/hts,shd->thd/dot_general | solution.py:65
  143.7 0.0 copy-start
  143.7 24.4 %all-gather.3.cloned.1.call-done = f32[64,128,128]{2,1,0:T(8,128)} async-done(((f32[8,128,128]{2,1,0:T(8,128)}), f32[64,128,128]{2,1,0:T(8,128)}) %all-gather.3.cloned.1.call-update) | async-done | bytes 4194320 | tf_op jit(solution)/shard_map/all_gather | solution.py:29
  168.1 2.7 %select_reduce_fusion = f32[8,128,128]{2,1,0:T(8,128)S(1)} fusion(f32[8,8,128,128]{3,2,1,0:T(8,128)} %bitcast.49, pred[8]{0:T(512)(128)(4,1)S(1)} %iota_compare_fusion.1), kind=kLoop, calls=%fused_computation.21 | loop fusion | flops 1966080 | bytes 4718600 | tf_op jit(solution)/shard_map/reduce_sum | solution.py:32
  170.8 0.0 copy-done
  170.8 0.0 copy-start.2
  170.8 4.5 %fusion.10 = (f32[1024,8]{0,1:T(8,128)S(1)}, f32[8,128,1024]{2,1,0:T(8,128)S(1)}) fusion(f32[8,128,1024]{2,1,0:T(8,128)} %fusion, f32[8,128,128]{2,1,0:T(8,128)S(1)} %select_reduce_fusion, bf16[1024,8,128]{2,1,0:T(8,128)(2,1)S(1)} %bitcast.45), kind=kOutput, calls=%fused_computation.16 | convolution fusion | flops 1614798848 | bytes 11042816 | tf_op jit(solution)/shard_map/thd,hde->the/dot_general | solution.py:47
  175.4 0.0 copy-done.2
  175.4 0.0 copy-start.1
  175.4 0.5 fusion.12
  175.9 2.6 %copy.29 = bf16[1024,1024]{1,0:T(8,128)(2,1)} copy(bf16[1024,1024]{0,1:T(8,128)(2,1)S(1)} %bitcast.46) | data formatting | bytes 4194304
  178.5 0.0 copy-done.1
  178.5 0.8 multiply_bitcast_fusion
  (2 shorter events, 0.0 us)
Async XLA Ops:
  21.1 29.9 %all-to-all-start.1 = ((bf16[256,4,1024]{2,0,1:T(8,128)(2,1)}), bf16[256,4,1024]{2,0,1:T(8,128)(2,1)S(1)}, u32[]{:S(2)}, u32[]{:S(2)}) async-start(bf16[256,4,1024]{2,0,1:T(8,128)(2,1)} %bitcast.42), calls=%async_computation.1 | async-start | bytes 4194304 | tf_op jit(solution)/shard_map/all_to_all | solution.py:21
  51.1 30.2 %all-to-all-start = ((bf16[256,4,1024]{0,2,1:T(8,128)(2,1)}), bf16[256,4,1024]{0,2,1:T(8,128)(2,1)}, u32[]{:S(2)}, u32[]{:S(2)}) async-start(bf16[256,4,1024]{0,2,1:T(8,128)(2,1)} %bitcast.41), calls=%async_computation | async-start | bytes 4194304 | tf_op jit(solution)/shard_map/all_to_all | solution.py:20
  55.5 112.5 %all-gather.3.cloned.1.call-start = ((), (), s32[]{:S(2)}) async-start(), calls=%async_computation.3 | async-start | bytes 4718592 | tf_op jit(solution)/shard_map/all_gather | solution.py:29
  96.6 30.2 %all-to-all-start.2 = ((bf16[256,4,1024]{2,0,1:T(8,128)(2,1)}), bf16[256,4,1024]{2,0,1:T(8,128)(2,1)}, u32[]{:S(2)}, u32[]{:S(2)}) async-start(bf16[256,4,1024]{2,0,1:T(8,128)(2,1)} %bitcast.39), calls=%async_computation.2 | async-start | bytes 4194304 | tf_op jit(solution)/shard_map/all_to_all | solution.py:19
  143.7 27.1 %copy-start = (bf16[128,8,8,128]{3,2,1,0:T(8,128)(2,1)S(1)}, bf16[128,8,8,128]{3,2,1,0:T(8,128)(2,1)}, u32[]{:S(2)}) copy-start(bf16[128,8,8,128]{3,2,1,0:T(8,128)(2,1)} %copy.35) | copy-start | bytes 6291460
  170.8 4.6 %copy-start.2 = (f32[1024]{0:T(1024)S(1)}, f32[1024]{0:T(1024)}, u32[]{:S(2)}) copy-start(f32[1024]{0:T(1024)} %param.9) | copy-start | bytes 12292
  175.4 3.0 %copy-start.1 = (f32[8,128,128]{2,1,0:T(8,128)S(1)}, f32[8,128,128]{2,1,0:T(8,128)}, u32[]{:S(2)}) copy-start(f32[8,128,128]{2,1,0:T(8,128)} %fusion.22) | copy-start | bytes 1572868
Sparse Core Ops, SparseCore 0:
  93.6 74.4 all-gather.2
where the time goes:
time: 187 us; the launch traced here: 186 us
  waiting for transfers between devices  91.7 us (49%)
  local copies, waits for them, and re-layouts  29.1 us (16%)
  matrix products  21 us (11%)
  other arithmetic  16.9 us (9%)
  between operations  14.2 us (8%)
  starting transfers between devices  13.4 us (7%)
    all_to_all x1, waiting for transfers between devices, per_device(): lax.all_to_all(spiked_query, 'head', split_axis=1, concat_axis=0, tiled=T...  25.2 us
    all_gather x1, waiting for transfers between devices, per_device(): piece = lax.all_gather(states[None], 'seq', axis=0, tiled=True)  24.4 us
    all_to_all x1, waiting for transfers between devices, per_device(): lax.all_to_all(spiked_value, 'head', split_axis=1, concat_axis=0, tiled=T...  21.6 us
    all_to_all x1, waiting for transfers between devices, per_device(): lax.all_to_all(spiked_key, 'head', split_axis=1, concat_axis=0, tiled=True)  20.5 us
    dot_general x1, matrix products, per_device(): jnp.einsum('hts,shd->thd', weights, value_tile, preferred_element_type=jn...  13.3 us
    mul x1, other arithmetic, per_device(): spiked_query = queries * count_query.astype(jnp.bfloat16)  12.5 us
    unnamed x9, local copies, waits for them, and re-layouts  8.06 us
    all_to_all x1, starting transfers between devices, per_device(): lax.all_to_all(spiked_query, 'head', split_axis=1, concat_axis=0, tiled=T...  4.64 us
  transfers between devices with their start and end apart: 4, of which 4 were waited for; matrix products, arithmetic and copies ran while one was open for 16% of the time, Pallas kernels for 0%

commit v1 on v0

v1 whole, which is shorter than its diff:
```python
import functools

import jax
import jax.numpy as jnp
from jax import lax
from jax.experimental import pallas as pl
from jax.experimental.pallas import tpu as pltpu
from jax.sharding import Mesh
from jax.sharding import PartitionSpec as P

HD = 128
SCORE_SCALE = HD ** (-0.5)
CORES = 2
VMEM_BYTES = 48 * 1024 * 1024


def params(n_axes):
    return pltpu.CompilerParams(
        dimension_semantics=("arbitrary",) * n_axes, vmem_limit_bytes=VMEM_BYTES
    )


def nine(spikes):
    return (spikes >= 9).astype(jnp.int32) + (spikes >= 18).astype(jnp.int32)


def three(code):
    return (code >= 3).astype(jnp.int32) + (code >= 6).astype(jnp.int32)


def count_of(spikes, name):
    value_count = nine(spikes)
    if name == "value":
        return value_count
    rest = spikes - 9 * value_count
    key_count = three(rest)
    if name == "key":
        return key_count
    return rest - 3 * key_count


def decode_kernel(names, width, core_ref, spikes_ref, *refs):
    sources = refs[: len(names)]
    outs = refs[len(names) :]
    core = core_ref[0]
    for side in range(CORES):
        of = core if side == 0 else 1 - core
        columns = pl.ds(pl.multiple_of(of * width, width), width)
        spikes = spikes_ref[:, columns]
        for index, name in enumerate(names):
            count = count_of(spikes, name).astype(jnp.float32).astype(jnp.bfloat16)
            outs[2 * index + side][...] = sources[index][:, columns] * count


def decode(core, spikes, operands, width):
    names = tuple(operands)
    rows, model = spikes.shape
    groups = model // (CORES * width)
    step = min(rows, 64)
    in_block = pl.BlockSpec((step, CORES * width), lambda r, g, core: (r, g))
    out_block = pl.BlockSpec((step, width), lambda r, g, core: (r, g))
    n_out = 2 * len(names)
    return pl.pallas_call(
        functools.partial(decode_kernel, names, width),
        out_shape=[jax.ShapeDtypeStruct((rows, groups * width), jnp.bfloat16)] * n_out,
        grid_spec=pltpu.PrefetchScalarGridSpec(
            num_scalar_prefetch=1,
            grid=(rows // step, groups),
            in_specs=[in_block] * (1 + len(names)),
            out_specs=[out_block] * n_out,
        ),
        compiler_params=params(2),
        cost_estimate=pl.CostEstimate(
            flops=rows * model * 8 * len(names),
            bytes_accessed=rows * model * 4 * (1 + len(names)),
            transcendentals=0,
        ),
        name="decode_" + "_".join(names),
    )(core, spikes, *operands.values())


def contract_rows(left, right):
    return lax.dot_general(
        left, right, (((0,), (0,)), ((), ())), preferred_element_type=jnp.float32
    )


def contract_columns(left, right):
    return lax.dot_general(
        left, right, (((1,), (1,)), ((), ())), preferred_element_type=jnp.float32
    )


def states_kernel(heads, key_ref, key_sib_ref, value_ref, value_sib_ref, out_ref):
    for h in range(heads):
        at = slice(h * HD, (h + 1) * HD)
        out_ref[h] = contract_rows(key_ref[:, at], value_ref[:, at]) + contract_rows(
            key_sib_ref[:, at], value_sib_ref[:, at]
        )


def chunk_states(key, key_sib, value, value_sib):
    rows, width = key.shape
    heads = width // HD
    step = min(heads, 4)
    block = pl.BlockSpec((rows, step * HD), lambda h: (0, h))
    return pl.pallas_call(
        functools.partial(states_kernel, step),
        out_shape=jax.ShapeDtypeStruct((heads, HD, HD), jnp.float32),
        grid=(heads // step,),
        in_specs=[block] * 4,
        out_specs=pl.BlockSpec((step, HD, HD), lambda h: (h, 0, 0)),
        compiler_params=params(1),
        cost_estimate=pl.CostEstimate(
            flops=4 * rows * HD * HD * heads,
            bytes_accessed=8 * rows * width + 4 * heads * HD * HD,
            transcendentals=0,
        ),
        name="chunk_states",
    )(key, key_sib, value, value_sib)


def prefix_kernel(block_tokens, states_ref, carry_ref, cache_ref):
    n_y, n_seq = states_ref.shape[:2]
    total = jnp.zeros(states_ref.shape[2:], jnp.float32)
    for s in range(n_seq):
        for y in range(n_y):
            carry_ref[y, s] = total
            total = total + states_ref[y, s]
        cache_ref[s] = total * ((s + 1) * block_tokens) ** (-0.5)


def prefix(states, block_tokens):
    n_y, n_seq, rows, _ = states.shape
    return pl.pallas_call(
        functools.partial(prefix_kernel, block_tokens),
        out_shape=[
            jax.ShapeDtypeStruct(states.shape, jnp.float32),
            jax.ShapeDtypeStruct((n_seq, rows, HD), jnp.float32),
        ],
        compiler_params=params(0),
        name="prefix",
    )(states)


def attend_kernel(
    heads, core_ref, q_ref, q_sib_ref, k_ref, k_sib_ref, v_ref, v_sib_ref, carry_ref, gain_ref, out_ref
):
    rows = q_ref.shape[0]
    is_first = jnp.broadcast_to(core_ref[0], (rows, HD)) == 0
    causal = lax.broadcasted_iota(jnp.int32, (rows, rows), 0) >= lax.broadcasted_iota(
        jnp.int32, (rows, rows), 1
    )

    def ordered(mine_ref, sib_ref, at):
        mine, sib = mine_ref[:, at], sib_ref[:, at]
        return jnp.where(is_first, mine, sib), jnp.where(is_first, sib, mine)

    def weigh(queries, keys, masked):
        scores = contract_columns(queries, keys) * SCORE_SCALE
        if masked:
            scores = jnp.where(causal, scores, 0.0)
        return scores.astype(jnp.bfloat16)

    def dot(left, right):
        return jnp.dot(left, right, preferred_element_type=jnp.float32)

    for h in range(heads):
        at = slice(h * HD, (h + 1) * HD)
        q_first, q_second = ordered(q_ref, q_sib_ref, at)
        k_first, k_second = ordered(k_ref, k_sib_ref, at)
        v_first, v_second = ordered(v_ref, v_sib_ref, at)
        carry = carry_ref[h] * SCORE_SCALE
        high = carry.astype(jnp.bfloat16)
        low = (carry - high.astype(jnp.float32)).astype(jnp.bfloat16)
        both = jnp.concatenate([high, low], axis=1)
        gain = gain_ref[:, at]

        def finish(raw, queries):
            carried = dot(queries, both)
            raw = raw + (carried[:, :HD] + carried[:, HD:])
            mean = jnp.mean(raw * raw, axis=-1, keepdims=True)
            return (raw * lax.rsqrt(mean + 1e-06) * gain).astype(jnp.bfloat16)

        raw_first = dot(weigh(q_first, k_first, True), v_first)
        out_ref[0, :rows, at] = finish(raw_first, q_first)
        raw_second = dot(weigh(q_second, k_first, False), v_first) + dot(
            weigh(q_second, k_second, True), v_second
        )
        out_ref[0, rows:, at] = finish(raw_second, q_second)


def attend(core, query, key, value, carry, gain, n_y):
    rows, width = key[0].shape
    heads = width // HD
    group = heads // n_y
    step = min(group, 2)
    steps = group // step
    block = pl.BlockSpec((rows, step * HD), lambda y, h, core: (0, y * steps + h))
    return pl.pallas_call(
        functools.partial(attend_kernel, step),
        out_shape=jax.ShapeDtypeStruct((n_y, 2 * rows, group * HD), jnp.bfloat16),
        grid_spec=pltpu.PrefetchScalarGridSpec(
            num_scalar_prefetch=1,
            grid=(n_y, steps),
            in_specs=[block] * 6
            + [
                pl.BlockSpec((step, HD, HD), lambda y, h, core: (y * steps + h, 0, 0)),
                pl.BlockSpec((1, step * HD), lambda y, h, core: (0, y * steps + h)),
            ],
            out_specs=pl.BlockSpec((1, 2 * rows, step * HD), lambda y, h, core: (y, 0, h)),
        ),
        compiler_params=params(2),
        cost_estimate=pl.CostEstimate(
            flops=heads * (12 * rows * rows * HD + 8 * rows * HD * HD),
            bytes_accessed=16 * rows * width + 4 * heads * HD * HD,
            transcendentals=0,
        ),
        name="attend",
    )(core, *query, *key, *value, carry, gain)


def per_device(n_seq, n_y, queries, keys, values, spikes, gain):
    rows, model = spikes.shape
    width = model // (n_y * CORES)
    chips = n_seq * n_y
    core = lax.axis_index("core").astype(jnp.int32).reshape(1)
    swap = [(0, 1), (1, 0)]

    key, key_out, value, value_out = decode(core, spikes, {"key": keys, "value": values}, width)
    key_sib = lax.ppermute(key_out, "core", swap)
    value_sib = lax.ppermute(value_out, "core", swap)
    query, query_out = decode(core, spikes, {"query": queries}, width)
    query_sib = lax.ppermute(query_out, "core", swap)

    states = chunk_states(key, key_sib, value, value_sib)
    heads = states.shape[0]
    pieces = states.reshape(chips, heads * HD // chips, HD)
    owned = lax.all_to_all(pieces, ("y", "seq"), split_axis=0, concat_axis=0, tiled=True)
    carry, cache = prefix(owned.reshape(n_y, n_seq, -1, HD), rows * CORES * n_y)
    carry = lax.all_to_all(
        carry.reshape(pieces.shape), ("y", "seq"), split_axis=0, concat_axis=0, tiled=True
    )
    gains = lax.all_gather(gain, "y", axis=0, tiled=True).reshape(1, n_y * width)
    attended = attend(
        core,
        (query, query_sib),
        (key, key_sib),
        (value, value_sib),
        carry.reshape(heads, HD, HD),
        gains,
        n_y,
    )
    attended = lax.all_to_all(attended, "y", split_axis=0, concat_axis=0, tiled=True)
    cache = lax.all_to_all(cache, "seq", split_axis=0, concat_axis=0, tiled=True)
    return attended.reshape(-1, width), cache.reshape(1, heads // n_y, HD, HD)


def solution(mesh):
    n_seq, n_head = mesh.shape["seq"], mesh.shape["head"]
    n_y = n_head // CORES
    split = Mesh(mesh.devices.reshape(n_seq, n_y, CORES), ("seq", "y", "core"))
    tokens = P(("seq", "y", "core"), None)
    return jax.shard_map(
        functools.partial(per_device, n_seq, n_y),
        mesh=split,
        in_specs=(tokens, tokens, tokens, tokens, P(("y", "core"))),
        out_specs=(P("seq", ("y", "core")), P("seq", ("y", "core"), None, None)),
        check_vma=False,
    )
```

time: 187 us -> 131 us (0.70)
  waiting for transfers between devices: 91.7 us -> 41.1 us
  blocking collectives: 0 us -> 39 us
  Pallas kernels: 0 us -> 26.3 us
  matrix products: 21 us -> 0 us
  local copies, waits for them, and re-layouts: 29.1 us -> 9.74 us
  other arithmetic: 16.9 us -> 0 us
  between operations: 14.2 us -> 0.72 us
    all_to_all x0 -> x1, blocking collectives: none -> 34.6 us  [per_device(): lax.all_to_all(pieces, ('y', 'seq'), split_axis=0, concat_axis=0, tiled=T...]
    all_to_all x3, waiting for transfers between devices: 67.3 us -> 37.4 us  [the longest x1 22 us: per_device(): lax.all_to_all(attended, 'y', split_axis=0, concat_axis=0, tiled=True)]
    pallas_call x0 -> x5, Pallas kernels: none -> 26.3 us  [the longest x2 13.5 us: decode(): pl.pallas_call(functools.partial(decode_kernel, names, width), out_shape=...]
    all_gather x1 -> x0, waiting for transfers between devices: 24.4 us -> none  [per_device(): piece = lax.all_gather(states[None], 'seq', axis=0, tiled=True)]
    dot_general x3 -> x0, matrix products: 21 us -> none  [the longest x1 13.3 us: per_device(): jnp.einsum('hts,shd->thd', weights, value_tile, preferred_element_type=jn...]
    mul x1 -> x0, other arithmetic: 12.5 us -> none  [per_device(): spiked_query = queries * count_query.astype(jnp.bfloat16)]
    all_to_all x3 -> x0, local copies, waits for them, and re-layouts: 9.22 us -> none  [the longest x1 4.55 us: per_device(): lax.all_to_all(spiked_key, 'head', split_axis=1, concat_axis=0, tiled=True)]
    reshape x2 -> x0, local copies, waits for them, and re-layouts: 7.7 us -> none  [the longest x1 4.46 us: per_device(): key_heads = key_block.reshape(block_rows, head_count, HD)]
  transfers between devices with their start and end apart: 4 -> 6, of which waited for: 4 -> 4; matrix products, arithmetic and copies ran while one was open for 16% -> 0% of each run, Pallas kernels for 0% -> 14%
where the time goes in v1:
time: 131 us; the launch traced here: 130 us
  waiting for transfers between devices  41.1 us (31%)
  blocking collectives  39 us (30%)
  Pallas kernels  26.3 us (20%)
  starting transfers between devices  12.9 us (10%)
  local copies, waits for them, and re-layouts  9.74 us (7%)
    all_to_all x1, blocking collectives, per_device(): lax.all_to_all(pieces, ('y', 'seq'), split_axis=0, concat_axis=0, tiled=T...  34.6 us
    all_to_all x1, waiting for transfers between devices, per_device(): lax.all_to_all(attended, 'y', split_axis=0, concat_axis=0, tiled=True)  22 us
    all_to_all x1, waiting for transfers between devices, per_device(): lax.all_to_all(carry.reshape(pieces.shape), ('y', 'seq'), split_axis=0, c...  15.4 us
    pallas_call x2, Pallas kernels, decode(): pl.pallas_call(functools.partial(decode_kernel, names, width), out_shape=...  13.5 us
    pallas_call x1, Pallas kernels, attend(): pl.pallas_call(functools.partial(attend_kernel, step), out_shape=jax.Shap...  10.9 us
    unnamed x16, local copies, waits for them, and re-layouts  9.74 us
    all_to_all x1, starting transfers between devices, per_device(): lax.all_to_all(carry.reshape(pieces.shape), ('y', 'seq'), split_axis=0, c...  4.35 us
    all_gather x1, blocking collectives, per_device(): lax.all_gather(gain, 'y', axis=0, tiled=True).reshape(1, n_y * width)  4.34 us
  transfers between devices with their start and end apart: 6, of which 4 were waited for; matrix products, arithmetic and copies ran while one was open for 0% of the time, Pallas kernels for 14%

profile of v1, /device:TPU:0, one launch (start us, length us, event | category | flops | bytes accessed | tf_op | source)
XLA Modules:
  0.0 129.8 jit_solution(6415204782374240494)
XLA Ops:
  0.6 6.7 %decode_key_value.1 = (bf16[256,2048]{1,0:T(8,128)(2,1)S(1)}, bf16[256,2048]{1,0:T(8,128)(2,1)S(1)}, bf16[256,2048]{1,0:T(8,128)(2,1)S(1)}, bf16[256,2048]{1,0:T(8,128)(2,1)S(1)}) custom-call(s32[1]{0:T(128)} %bitcast.core_ref, s32[256,4096]{1,0:T(8,128)} %spikes_ref.3, bf16[256,4096]{1,0:T(8,128)(2,1)} %refs_0_.3, bf16[256,4096]{1,0:T(8,128)(2,1)} %refs_1_.1), custom_call_target="tpu_custom_call" | custom-call | flops 16777216 | bytes 12582912 | tf_op jit(solution)/shard_map/decode_key_value/pallas_call | solution.py:63
  7.3 0.5 collective-permute-start.1
  7.8 0.1 collective-permute-start.2
  7.9 2.2 %collective-permute-done.1.key_sib_ref.k_sib_ref = bf16[256,2048]{1,0:T(8,128)(2,1)S(1)} collective-permute-done((bf16[256,2048]{1,0:T(8,128)(2,1)S(1)}, bf16[256,2048]{1,0:T(8,128)(2,1)S(1)}, u32[]{:S(2)}, u32[]{:S(2)}) %collective-permute-start.1) | collective-permute-done | bytes 1048608 | tf_op jit(solution)/shard_map/ppermute | solution.py:231
  10.1 1.5 %collective-permute-done.2.value_sib_ref.v_sib_ref = bf16[256,2048]{1,0:T(8,128)(2,1)S(1)} collective-permute-done((bf16[256,2048]{1,0:T(8,128)(2,1)S(1)}, bf16[256,2048]{1,0:T(8,128)(2,1)S(1)}, u32[]{:S(2)}, u32[]{:S(2)}) %collective-permute-start.2) | collective-permute-done | bytes 1048608 | tf_op jit(solution)/shard_map/ppermute | solution.py:232
  11.6 1.8 %chunk_states.1 = f32[16,128,128]{2,1,0:T(8,128)S(1)} custom-call(bf16[256,2048]{1,0:T(8,128)(2,1)S(1)} %get-tuple-element.12.key_ref.k_ref, bf16[256,2048]{1,0:T(8,128)(2,1)S(1)} %collective-permute-done.1.key_sib_ref.k_sib_ref, bf16[256,2048]{1,0:T(8,128)(2,1)S(1)} %get-tuple-element.14.value_ref.v_ref, ...), custom_call_target="tpu_custom_call" | custom-call | flops 268435456 | bytes 5242880 | tf_op jit(solution)/shard_map/chunk_states/pallas_call | solution.py:107
  13.4 0.0 copy-start
  13.4 1.0 copy-done
  14.4 34.6 %all_to_all.20 = f32[16,128,128]{2,1,0:T(8,128)S(1)} all-to-all(f32[16,128,128]{2,1,0:T(8,128)S(1)} %chunk_states.1), channel_id=1, replica_groups=mesh['seq'=8,'y'=2,'core'=2] {'y','seq'}, dimensions={0} | all-to-all | bytes 2097152 | tf_op jit(solution)/shard_map/all_to_all | solution.py:239
  49.0 0.1 prefix.1
  49.1 0.0 copy-start.2
  49.2 1.0 copy-done.2
  50.1 0.0 copy-start.5
  50.1 0.8 copy-done.5
  50.9 4.3 %all-to-all-start.1 = ((f32[16,128,128]{2,1,0:T(8,128)}), f32[16,128,128]{2,1,0:T(8,128)}, u32[]{:S(2)}, u32[]{:S(2)}) async-start(f32[16,128,128]{2,1,0:T(8,128)} %bitcast.7), calls=%async_computation.1 | async-start | bytes 2097152 | tf_op jit(solution)/shard_map/all_to_all | solution.py:241
  55.3 0.0 copy-start.1
  55.3 1.6 %copy-done.1 = bf16[256,4096]{1,0:T(8,128)(2,1)S(1)} copy-done((bf16[256,4096]{1,0:T(8,128)(2,1)S(1)}, bf16[256,4096]{1,0:T(8,128)(2,1)}, u32[]{:S(2)}) %copy-start.1) | copy-done | bytes 2097176
  56.9 0.0 copy-start.6
  56.9 6.8 %decode_query.1 = (bf16[256,2048]{1,0:T(8,128)(2,1)S(1)}, bf16[256,2048]{1,0:T(8,128)(2,1)}) custom-call(s32[1]{0:T(128)} %bitcast.core_ref, s32[256,4096]{1,0:T(8,128)} %spikes_ref.3, bf16[256,4096]{1,0:T(8,128)(2,1)S(1)} %copy-done.1), custom_call_target="tpu_custom_call" | custom-call | flops 8388608 | bytes 8388608 | tf_op jit(solution)/shard_map/decode_query/pallas_call | solution.py:63
  63.7 0.0 copy-start.3
  63.7 1.0 copy-done.3
  64.7 0.0 collective-permute-start
  64.7 15.4 %all-to-all-done.1.carry_ref = f32[16,128,128]{2,1,0:T(8,128)} async-done(((f32[16,128,128]{2,1,0:T(8,128)}), f32[16,128,128]{2,1,0:T(8,128)}, u32[]{:S(2)}, u32[]{:S(2)}) %all-to-all-start.1) | async-done | bytes 1048608 | tf_op jit(solution)/shard_map/all_to_all | solution.py:241
  80.1 4.2 %all-to-all-start.3 = ((f32[8,128,128]{2,1,0:T(8,128)}), f32[8,128,128]{2,1,0:T(8,128)}, u32[]{:S(2)}, u32[]{:S(2)}) async-start(f32[8,128,128]{2,1,0:T(8,128)} %copy-done.5), calls=%async_computation.3 | async-start | bytes 1048576 | tf_op jit(solution)/shard_map/all_to_all | solution.py:255
  84.3 0.0 copy-done.6
  84.3 4.3 %all_gather.3 = f32[2048]{0:T(1024)S(1)} all-gather(f32[1024]{0:T(1024)S(1)} %copy-done.6), channel_id=1, replica_groups=mesh['seq'=8,'y'=2,'core'=2] {'y'}, dimensions={0}, use_global_device_ids=true | all-gather | bytes 12288 | tf_op jit(solution)/shard_map/all_gather | solution.py:244
  88.6 0.0 collective-permute-done.q_sib_ref
  88.6 0.0 copy-start.4
  88.6 1.2 copy-done.4
  89.9 10.9 %attend.1 = bf16[2,512,1024]{2,1,0:T(8,128)(2,1)} custom-call(s32[1]{0:T(128)} %bitcast.core_ref, bf16[256,2048]{1,0:T(8,128)(2,1)S(1)} %copy-done.4, bf16[256,2048]{1,0:T(8,128)(2,1)} %collective-permute-done.q_sib_ref, bf16[256,2048]{1,0:T(8,128)(2,1)S(1)} %get-tuple-element.12.key_ref.k_ref, ...), custom_call_target="tpu_custom_call" | custom-call | flops 2147483648 | bytes 9437184 | tf_op jit(solution)/shard_map/attend/pallas_call | solution.py:200
  100.8 0.0 all-to-all-done.3
  100.8 3.8 %all-to-all-start.2 = ((bf16[2,512,1024]{2,1,0:T(8,128)(2,1)}), bf16[2,512,1024]{2,1,0:T(8,128)(2,1)S(1)}, u32[]{:S(2)}, u32[]{:S(2)}) async-start(bf16[2,512,1024]{2,1,0:T(8,128)(2,1)} %attend.1), calls=%async_computation.2 | async-start | bytes 4194304 | tf_op jit(solution)/shard_map/all_to_all | solution.py:254
  104.6 22.0 %all-to-all-done.2 = bf16[2,512,1024]{2,1,0:T(8,128)(2,1)S(1)} async-done(((bf16[2,512,1024]{2,1,0:T(8,128)(2,1)}), bf16[2,512,1024]{2,1,0:T(8,128)(2,1)S(1)}, u32[]{:S(2)}, u32[]{:S(2)}) %all-to-all-start.2) | async-done | bytes 2097184 | tf_op jit(solution)/shard_map/all_to_all | solution.py:254
  126.6 1.3 %copy.9 = bf16[1024,1024]{1,0:T(8,128)(2,1)} copy(bf16[1024,1024]{1,0:T(8,128)(2,1)S(1)} %bitcast.9) | data formatting | bytes 4194304
  127.9 1.9 %copy.10 = f32[1,8,128,128]{3,2,1,0:T(8,128)} copy(f32[1,8,128,128]{3,2,1,0:T(8,128)} %bitcast.5) | data formatting | bytes 1048576
Async XLA Ops:
  7.3 2.8 %collective-permute-start.1 = (bf16[256,2048]{1,0:T(8,128)(2,1)S(1)}, bf16[256,2048]{1,0:T(8,128)(2,1)S(1)}, u32[]{:S(2)}, u32[]{:S(2)}) collective-permute-start(bf16[256,2048]{1,0:T(8,128)(2,1)S(1)} %get-tuple-element.13), channel_id=1, source_target_pairs={{0,1},{1,0},{2,3},{3,2},{4,5},{5,4},{6,7},{7,6},{8,9},{9,8},{10,11... | collective-permute-start | bytes 3145736 | tf_op jit(solution)/shard_map/ppermute | solution.py:231
  7.8 3.8 %collective-permute-start.2 = (bf16[256,2048]{1,0:T(8,128)(2,1)S(1)}, bf16[256,2048]{1,0:T(8,128)(2,1)S(1)}, u32[]{:S(2)}, u32[]{:S(2)}) collective-permute-start(bf16[256,2048]{1,0:T(8,128)(2,1)S(1)} %get-tuple-element.15), channel_id=1, source_target_pairs={{0,1},{1,0},{2,3},{3,2},{4,5},{5,4},{6,7},{7,6},{8,9},{9,8},{10,11... | collective-permute-start | bytes 3145736 | tf_op jit(solution)/shard_map/ppermute | solution.py:232
  13.4 1.0 copy-start
  49.1 1.0 copy-start.2
  50.1 0.8 copy-start.5
  50.9 29.2 %all-to-all-start.1 = ((f32[16,128,128]{2,1,0:T(8,128)}), f32[16,128,128]{2,1,0:T(8,128)}, u32[]{:S(2)}, u32[]{:S(2)}) async-start(f32[16,128,128]{2,1,0:T(8,128)} %bitcast.7), calls=%async_computation.1 | async-start | bytes 2097152 | tf_op jit(solution)/shard_map/all_to_all | solution.py:241
  55.3 1.6 %copy-start.1 = (bf16[256,4096]{1,0:T(8,128)(2,1)S(1)}, bf16[256,4096]{1,0:T(8,128)(2,1)}, u32[]{:S(2)}) copy-start(bf16[256,4096]{1,0:T(8,128)(2,1)} %refs_0_.2) | copy-start | bytes 6291460
  56.9 27.4 %copy-start.6 = (f32[1024]{0:T(1024)S(1)}, f32[1024]{0:T(1024)}, u32[]{:S(2)}) copy-start(f32[1024]{0:T(1024)} %param.9) | copy-start | bytes 12292
  63.7 1.0 copy-start.3
  64.7 23.9 %collective-permute-start = (bf16[256,2048]{1,0:T(8,128)(2,1)}, bf16[256,2048]{1,0:T(8,128)(2,1)}, u32[]{:S(2)}, u32[]{:S(2)}) collective-permute-start(bf16[256,2048]{1,0:T(8,128)(2,1)} %get-tuple-element.11), channel_id=1, source_target_pairs={{0,1},{1,0},{2,3},{3,2},{4,5},{5,4},{6,7},{7,6},{8,9},{9,8},{10,11... | collective-permute-start | bytes 3145736 | tf_op jit(solution)/shard_map/ppermute | solution.py:234
  80.1 20.7 %all-to-all-start.3 = ((f32[8,128,128]{2,1,0:T(8,128)}), f32[8,128,128]{2,1,0:T(8,128)}, u32[]{:S(2)}, u32[]{:S(2)}) async-start(f32[8,128,128]{2,1,0:T(8,128)} %copy-done.5), calls=%async_computation.3 | async-start | bytes 1048576 | tf_op jit(solution)/shard_map/all_to_all | solution.py:255
  88.6 1.2 copy-start.4
  100.8 25.8 %all-to-all-start.2 = ((bf16[2,512,1024]{2,1,0:T(8,128)(2,1)}), bf16[2,512,1024]{2,1,0:T(8,128)(2,1)S(1)}, u32[]{:S(2)}, u32[]{:S(2)}) async-start(bf16[2,512,1024]{2,1,0:T(8,128)(2,1)} %attend.1), calls=%async_computation.2 | async-start | bytes 4194304 | tf_op jit(solution)/shard_map/all_to_all | solution.py:254

commit v2 on v0

v2 whole, which is shorter than its diff:
```python
import functools

import jax
import jax.numpy as jnp
from jax import lax
from jax.experimental import pallas as pl
from jax.experimental.pallas import tpu as pltpu
from jax.sharding import Mesh
from jax.sharding import PartitionSpec as P

HD = 128
SCORE_SCALE = HD ** (-0.5)
CORES = 2
VMEM_BYTES = 24 * 1024 * 1024
PAD = 16
TOP = 32767.0

VMEM = pl.BlockSpec(memory_space=pltpu.VMEM)
SMEM = pl.BlockSpec(memory_space=pltpu.SMEM)


def params(n_axes=0):
    return pltpu.CompilerParams(
        dimension_semantics=("arbitrary",) * n_axes or None, vmem_limit_bytes=VMEM_BYTES
    )


def cost(flops, bytes_accessed):
    return pl.CostEstimate(flops=flops, bytes_accessed=bytes_accessed, transcendentals=0)


class Plan:
    def __init__(self, mesh, rows, model):
        n_seq, n_head = mesh.shape["seq"], mesh.shape["head"]
        self.n_y = n_head // CORES
        self.width = model // n_head
        group = self.width // HD
        self.n_inner = 2 if n_seq % 2 == 0 and group % 2 == 0 else 1
        self.n_outer = n_seq // self.n_inner
        self.halves = 2 if group // self.n_inner % 2 == 0 else 1
        self.each = group // (self.n_inner * self.halves)
        self.plane = self.n_inner * self.n_y
        self.rows = rows
        self.block = rows * n_head
        self.half_width = self.width // self.halves


def decode_kernel(names, *refs):
    n = len(names)
    for side in range(CORES):
        spikes = refs[side][...].astype(jnp.float32).astype(jnp.bfloat16)
        one, two = jnp.ones_like(spikes), jnp.full_like(spikes, 2)
        zero = jnp.zeros_like(spikes)

        def ternary(code, unit):
            return jnp.where(code >= 2 * unit, two, jnp.where(code >= unit, one, zero))

        counts = {"value": ternary(spikes, 9)}
        if "value" not in names or n > 1:
            rest = spikes - 9 * counts["value"]
            counts["key"] = ternary(rest, 3)
            if "query" in names:
                counts["query"] = rest - 3 * counts["key"]
        for index, name in enumerate(names):
            at = 2 * index + side
            refs[2 + 2 * n + at][...] = refs[2 + at][...] * counts[name]


def decode(plan, place, spikes, operands, half):
    names = tuple(operands)
    rows, model = spikes.shape
    step = min(rows, 128)
    width = plan.half_width

    def block(sibling):
        def index(r, y, place):
            core = 1 - place[0] if sibling else place[0]
            return r, (y * CORES + core) * plan.halves + half

        return pl.BlockSpec((step, width), index)

    def kernel(place_ref, *refs):
        decode_kernel(names, *refs)

    n_out = 2 * len(names)
    arrays = [a for a in (spikes, *operands.values()) for _ in range(2)]
    return pl.pallas_call(
        kernel,
        out_shape=[jax.ShapeDtypeStruct((rows, plan.n_y * width), jnp.bfloat16)] * n_out,
        grid_spec=pltpu.PrefetchScalarGridSpec(
            num_scalar_prefetch=1,
            grid=(rows // step, plan.n_y),
            in_specs=[block(False), block(True)] * (1 + len(names)),
            out_specs=[pl.BlockSpec((step, width), lambda r, y, place: (r, y))] * n_out,
        ),
        compiler_params=params(2),
        cost_estimate=cost(rows * model * 4, rows * model * (2 + 2 * len(names))),
        name="decode_" + "_".join(names) + f"_{half}",
    )(place, *arrays)


def contract_rows(left, right):
    return lax.dot_general(
        left, right, (((0,), (0,)), ((), ())), preferred_element_type=jnp.float32
    )


def contract_columns(left, right):
    return lax.dot_general(
        left, right, (((1,), (1,)), ((), ())), preferred_element_type=jnp.float32
    )


def code(states, ref):
    line = lax.broadcasted_iota(jnp.int32, (PAD, HD), 0)
    exponents = jnp.zeros((PAD, HD), jnp.float32)
    for i, state in enumerate(states):
        top = jnp.max(jnp.abs(state), axis=0, keepdims=True)
        exponent = jnp.floor(jnp.log2(jnp.maximum(top, 1e-30))) + 1
        scaled = jnp.round(state * jnp.exp2(15 - exponent))
        scaled = jnp.clip(scaled, -TOP, TOP)
        ref[i * HD : (i + 1) * HD] = scaled.astype(jnp.int32).astype(jnp.int16)
        exponents = jnp.where(line == i, exponent, exponents)
    ref[len(states) * HD :] = exponents.astype(jnp.int32).astype(jnp.int16)


def decoded(ref, each):
    exponents = ref[each * HD :].astype(jnp.int32).astype(jnp.float32)
    return [
        ref[i * HD : (i + 1) * HD].astype(jnp.int32).astype(jnp.float32)
        * jnp.exp2(exponents[i : i + 1] - 15)
        for i in range(each)
    ]


def coded_shape(plan):
    return jax.ShapeDtypeStruct((plan.each * HD + PAD, HD), jnp.int16)


def states_shape(plan, *lead):
    return jax.ShapeDtypeStruct((*lead, plan.each, HD, HD), jnp.float32)


def owned_columns(plan, place_ref, offset, i):
    x = place_ref[1] ^ (offset // plan.n_y)
    y = place_ref[2] ^ (offset % plan.n_y)
    start = ((y * plan.n_inner + x) * plan.each + i) * HD
    return pl.ds(pl.multiple_of(start, HD), HD)


def chunk_states(plan, place, key, value):
    def kernel(place_ref, k_ref, k_sib_ref, v_ref, v_sib_ref, own_ref, first_ref, *send_refs):
        is_first = jnp.full((HD, HD), place_ref[0], jnp.int32) == 0
        for offset in range(plan.plane):
            states = []
            for i in range(plan.each):
                at = owned_columns(plan, place_ref, offset, i)
                mine = contract_rows(v_ref[:, at], k_ref[:, at])
                sib = contract_rows(v_sib_ref[:, at], k_sib_ref[:, at])
                first_ref[offset, i] = jnp.where(is_first, mine, sib)
                states.append(mine + sib)
            if offset:
                code(states, send_refs[offset - 1])
            else:
                for i, state in enumerate(states):
                    own_ref[i] = state

    heads = plan.plane * plan.each
    return pl.pallas_call(
        kernel,
        out_shape=[states_shape(plan), states_shape(plan, plan.plane)]
        + [coded_shape(plan)] * (plan.plane - 1),
        in_specs=[SMEM] + [VMEM] * 4,
        out_specs=[VMEM] * (1 + plan.plane),
        compiler_params=params(),
        cost_estimate=cost(
            4 * plan.rows * HD * HD * heads, 8 * plan.rows * HD * heads + 6 * heads * HD * HD
        ),
        name="chunk_states",
    )(place, *key, *value)


def level_states(plan, own, others):
    def kernel(own_ref, *refs):
        total = [own_ref[i] for i in range(plan.each)]
        for ref in refs[:-1]:
            total = [a + b for a, b in zip(total, decoded(ref, plan.each))]
        code(total, refs[-1])

    return pl.pallas_call(
        kernel,
        out_shape=coded_shape(plan),
        in_specs=[VMEM] * plan.plane,
        out_specs=VMEM,
        compiler_params=params(),
        cost_estimate=cost(0, plan.plane * plan.each * HD * HD * 2),
        name="level_states",
    )(own, *others)


def carries(plan, place, own, others, levels):
    n_others, n_levels = len(others), len(levels)

    def kernel(place_ref, own_ref, *refs):
        other_refs = refs[:n_others]
        level_refs = refs[n_others : n_others + n_levels]
        carry_refs = refs[n_others + n_levels : n_others + n_levels + plan.plane]
        cache_refs = refs[n_others + n_levels + plan.plane :]
        x, y, level = place_ref[1], place_ref[2], place_ref[3]
        here = x * plan.n_y + y
        earlier = [jnp.zeros((HD, HD), jnp.float32)] * plan.each
        for ref in level_refs:
            earlier = [a + b for a, b in zip(earlier, decoded(ref, plan.each))]
        states = [[own_ref[i] for i in range(plan.each)]]
        states += [decoded(ref, plan.each) for ref in other_refs]

        def add(totals, keep_of):
            for offset, terms in enumerate(states):
                keep = jnp.full((HD, HD), keep_of(here ^ offset), jnp.int32) == 1
                totals = [t + jnp.where(keep, s, 0.0) for t, s in zip(totals, terms)]
            return totals

        for offset, ref in enumerate(carry_refs):
            to = here ^ offset
            code(add(earlier, lambda chip: (chip < to).astype(jnp.int32)), ref)
        for offset, ref in enumerate(cache_refs):
            to = x ^ offset
            block = level * plan.n_inner + to
            seen = jnp.full((1, HD), (block + 1) * plan.block, jnp.int32).astype(jnp.float32)
            totals = add(earlier, lambda chip: (chip // plan.n_y <= to).astype(jnp.int32))
            for i, total in enumerate(totals):
                ref[i] = total.T * lax.rsqrt(seen)

    return pl.pallas_call(
        kernel,
        out_shape=[coded_shape(plan)] * plan.plane + [states_shape(plan)] * plan.n_inner,
        in_specs=[SMEM] + [VMEM] * (1 + n_others + n_levels),
        out_specs=[VMEM] * (plan.plane + plan.n_inner),
        compiler_params=params(),
        cost_estimate=cost(0, (plan.plane * 4 + n_levels) * plan.each * HD * HD * 2),
        name="carries",
    )(place, own, *others, *levels)


def attend(plan, place, query, key, value, carry, first, gain, half, offset_y):
    rows = plan.rows

    def kernel(
        place_ref, q_ref, q_sib_ref, k_ref, k_sib_ref, v_ref, v_sib_ref, first_ref, gain_ref, *refs
    ):
        core = place_ref[0]
        out_ref = refs[-1]
        causal = lax.broadcasted_iota(jnp.int32, (rows, rows), 0) >= lax.broadcasted_iota(
            jnp.int32, (rows, rows), 1
        )
        is_second = jnp.full((HD, HD), core, jnp.int32) == 1

        def attended(q_ref, k_ref, v_ref, at, carried, gain):
            queries = q_ref[:, at]
            scores = contract_columns(queries, k_ref[:, at]) * SCORE_SCALE
            weights = jnp.where(causal, scores, 0.0).astype(jnp.bfloat16)
            raw = jnp.dot(weights, v_ref[:, at], preferred_element_type=jnp.float32)
            carried = carried * SCORE_SCALE
            high = carried.astype(jnp.bfloat16)
            low = (carried - high.astype(jnp.float32)).astype(jnp.bfloat16)
            both = contract_columns(queries, jnp.concatenate([high, low], axis=0))
            raw = raw + (both[:, :HD] + both[:, HD:])
            mean = jnp.mean(raw * raw, axis=-1, keepdims=True)
            return (raw * lax.rsqrt(mean + 1e-06) * gain).astype(jnp.bfloat16)

        for offset_x in range(plan.n_inner):
            offset = offset_x * plan.n_y + offset_y
            x = place_ref[1] ^ offset_x
            carry_states = decoded(refs[offset_x], plan.each)
            for i in range(plan.each):
                at = owned_columns(plan, place_ref, offset, i)
                start = (x * plan.each + i) * HD
                in_group = pl.ds(pl.multiple_of(half * plan.half_width + start, HD), HD)
                out_at = pl.ds(pl.multiple_of(start, HD), HD)
                gain = gain_ref[:, in_group]
                first = first_ref[offset, i]
                mine = carry_states[i] + jnp.where(is_second, first, 0.0)
                sib = carry_states[i] + jnp.where(is_second, 0.0, first)
                out_ref[pl.ds(pl.multiple_of(core * rows, rows), rows), out_at] = attended(
                    q_ref, k_ref, v_ref, at, mine, gain
                )
                out_ref[pl.ds(pl.multiple_of((1 - core) * rows, rows), rows), out_at] = attended(
                    q_sib_ref, k_sib_ref, v_sib_ref, at, sib, gain
                )

    heads = plan.n_inner * plan.each
    return pl.pallas_call(
        kernel,
        out_shape=jax.ShapeDtypeStruct((CORES * rows, plan.half_width), jnp.bfloat16),
        in_specs=[SMEM] + [VMEM] * (8 + plan.n_inner),
        out_specs=VMEM,
        compiler_params=params(),
        cost_estimate=cost(
            heads * (8 * rows * rows * HD + 8 * rows * HD * HD), 16 * rows * heads * HD
        ),
        name=f"attend_{half}_{offset_y}",
    )(place, *query, *key, *value, first, gain, *carry)


def assemble(plan, place, parts):
    rows = CORES * plan.rows

    def kernel(place_ref, *refs):
        out_ref = refs[-1]
        for offset_y in range(plan.n_y):
            y = place_ref[2] ^ offset_y
            for half in range(plan.halves):
                at = slice(half * plan.half_width, (half + 1) * plan.half_width)
                part = refs[offset_y * plan.halves + half]
                out_ref[pl.ds(pl.multiple_of(y * rows, rows), rows), at] = part[...]

    return pl.pallas_call(
        kernel,
        out_shape=jax.ShapeDtypeStruct((plan.n_y * rows, plan.width), jnp.bfloat16),
        in_specs=[SMEM] + [VMEM] * (plan.n_y * plan.halves),
        out_specs=VMEM,
        compiler_params=params(),
        name="assemble",
    )(place, *[part for halves in parts for part in halves])


def assemble_cache(plan, place, parts):
    heads = plan.halves * plan.n_inner * plan.each

    def kernel(place_ref, *refs):
        out_ref = refs[-1]
        for half in range(plan.halves):
            for offset_x in range(plan.n_inner):
                x = place_ref[1] ^ offset_x
                start = (half * plan.n_inner + x) * plan.each
                out_ref[0, pl.ds(start, plan.each)] = refs[half * plan.n_inner + offset_x][...]

    return pl.pallas_call(
        kernel,
        out_shape=jax.ShapeDtypeStruct((1, heads, HD, HD), jnp.float32),
        in_specs=[SMEM] + [VMEM] * (plan.halves * plan.n_inner),
        out_specs=VMEM,
        compiler_params=params(),
        name="assemble_cache",
    )(place, *[part for offsets in parts for part in offsets])


def per_device(plan, queries, keys, values, spikes, gain):
    place = jnp.stack([lax.axis_index(a) for a in ("core", "inner", "y", "outer")]).astype(jnp.int32)
    halves = range(plan.halves)

    def swap(array, axes, offset, size):
        return lax.ppermute(array, axes, [(i, i ^ offset) for i in range(size)])

    def in_level(array, offset):
        return swap(array, ("inner", "y"), offset, plan.plane)

    def to_later(array, distance):
        pairs = [(i, i + distance) for i in range(plan.n_outer - distance)]
        return lax.ppermute(array, "outer", pairs)

    def spiked(operands, half):
        arrays = decode(plan, place, spikes, operands, half)
        return [
            (arrays[2 * i], swap(arrays[2 * i + 1], "core", 1, CORES)) for i in range(len(operands))
        ]

    gain = gain.reshape(1, plan.width)
    gains = [gain] + [swap(gain, "y", o, plan.n_y) for o in range(1, plan.n_y)]
    pairs = [spiked({"key": keys, "value": values}, half) for half in halves]
    states = []
    for half in halves:
        own, first, *sends = chunk_states(plan, place, *pairs[half])
        others = [in_level(a, o) for o, a in enumerate(sends, 1)]
        states.append((own, first, others))
    query = [spiked({"query": queries}, half)[0] for half in halves]
    levels = []
    for half in halves:
        own, _, others = states[half]
        level = level_states(plan, own, others)
        levels.append([to_later(level, d) for d in range(1, plan.n_outer)])
    carry, caches = [], []
    for half in halves:
        own, _, others = states[half]
        outs = carries(plan, place, own, others, levels[half])
        mine, *sends = outs[: plan.plane]
        carry.append([mine] + [in_level(a, o) for o, a in enumerate(sends, 1)])
        cache, *sends = outs[plan.plane :]
        caches.append([cache] + [swap(a, "inner", o, plan.n_inner) for o, a in enumerate(sends, 1)])
    parts = [[None] * plan.halves for _ in range(plan.n_y)]
    for offset_y in (*range(1, plan.n_y), 0):
        for half in halves:
            part = attend(
                plan,
                place,
                query[half],
                *pairs[half],
                carry[half][offset_y :: plan.n_y],
                states[half][1],
                gains[offset_y],
                half,
                offset_y,
            )
            parts[offset_y][half] = swap(part, "y", offset_y, plan.n_y) if offset_y else part
    return assemble(plan, place, parts), assemble_cache(plan, place, caches)


def solution(mesh):
    tokens = P(("outer", "inner", "y", "core"), None)
    seq, head = ("outer", "inner"), ("y", "core")

    def whole(queries, keys, values, spikes, gain):
        plan = Plan(mesh, spikes.shape[0] // mesh.size, spikes.shape[1])
        sizes = (plan.n_outer, plan.n_inner, plan.n_y, CORES)
        split = Mesh(mesh.devices.reshape(sizes), ("outer", "inner", "y", "core"))
        return jax.shard_map(
            functools.partial(per_device, plan),
            mesh=split,
            in_specs=(tokens, tokens, tokens, tokens, P(head)),
            out_specs=(P(seq, head), P(seq, head, None, None)),
            check_vma=False,
        )(queries, keys, values, spikes, gain)

    return whole
```

time: 187 us -> 80.3 us (0.43)
  waiting for transfers between devices: 91.7 us -> 9.96 us
  starting transfers between devices: 13.4 us -> 40.4 us
  local copies, waits for them, and re-layouts: 29.1 us -> 5.38 us
  Pallas kernels: 0 us -> 23.3 us
  matrix products: 21 us -> 0 us
  other arithmetic: 16.9 us -> 0.08 us
  between operations: 14.2 us -> 0.9 us
    all_to_all x3 -> x0, waiting for transfers between devices: 67.3 us -> none  [the longest x1 25.2 us: per_device(): lax.all_to_all(spiked_query, 'head', split_axis=1, concat_axis=0, tiled=T...]
    ppermute x0 -> x29, starting transfers between devices: none -> 40.4 us  [the longest x23 22.6 us: swap(): return lax.ppermute(array, axes, [(i, i ^ offset) for i in range(size)])]
    all_gather x1 -> x0, waiting for transfers between devices: 24.4 us -> none  [per_device(): piece = lax.all_gather(states[None], 'seq', axis=0, tiled=True)]
    pallas_call x0 -> x16, Pallas kernels: none -> 23.3 us  [the longest x4 7.5 us: attend(): pl.pallas_call(kernel, out_shape=jax.ShapeDtypeStruct((CORES * rows, plan...]
    dot_general x3 -> x0, matrix products: 21 us -> none  [the longest x1 13.3 us: per_device(): jnp.einsum('hts,shd->thd', weights, value_tile, preferred_element_type=jn...]
    all_to_all x3 -> x0, starting transfers between devices: 13.3 us -> none  [the longest x1 4.64 us: per_device(): lax.all_to_all(spiked_query, 'head', split_axis=1, concat_axis=0, tiled=T...]
    mul x1 -> x0, other arithmetic: 12.5 us -> none  [per_device(): spiked_query = queries * count_query.astype(jnp.bfloat16)]
    ppermute x0 -> x29, waiting for transfers between devices: none -> 9.96 us  [the longest x23 9.95 us: swap(): return lax.ppermute(array, axes, [(i, i ^ offset) for i in range(size)])]
  transfers between devices with their start and end apart: 4 -> 29, of which waited for: 4 -> 7; matrix products, arithmetic and copies ran while one was open for 16% -> 0% of each run, Pallas kernels for 0% -> 24%
where the time goes in v2:
time: 80.3 us; the launch traced here: 80 us
  starting transfers between devices  40.4 us (50%)
  Pallas kernels  23.3 us (29%)
  waiting for transfers between devices  9.96 us (12%)
  local copies, waits for them, and re-layouts  5.38 us (7%)
  between operations  0.9 us (1%)
    ppermute x23, starting transfers between devices, swap(): return lax.ppermute(array, axes, [(i, i ^ offset) for i in range(size)])  22.6 us
    ppermute x6, starting transfers between devices, to_later(): return lax.ppermute(array, 'outer', pairs)  17.8 us
    ppermute x23, waiting for transfers between devices, swap(): return lax.ppermute(array, axes, [(i, i ^ offset) for i in range(size)])  9.95 us
    pallas_call x4, Pallas kernels, attend(): pl.pallas_call(kernel, out_shape=jax.ShapeDtypeStruct((CORES * rows, plan...  7.5 us
    pallas_call x4, Pallas kernels, decode(): pl.pallas_call(kernel, out_shape=[jax.ShapeDtypeStruct((rows, plan.n_y *...  7.49 us
    unnamed x10, local copies, waits for them, and re-layouts  5.38 us
    pallas_call x2, Pallas kernels, chunk_states(): pl.pallas_call(kernel, out_shape=[states_shape(plan), states_shape(plan,...  2.83 us
    pallas_call x1, Pallas kernels, assemble(): pl.pallas_call(kernel, out_shape=jax.ShapeDtypeStruct((plan.n_y * rows, p...  2.02 us
  transfers between devices with their start and end apart: 29, of which 7 were waited for; matrix products, arithmetic and copies ran while one was open for 0% of the time, Pallas kernels for 24%

profile of v2, /device:TPU:0, one launch (start us, length us, event | category | flops | bytes accessed | tf_op | source)
XLA Modules:
  0.0 80.0 jit_solution(4765607496488266798)
XLA Ops:
  0.6 0.1 pad_add_fusion.place_ref
  0.7 2.2 %copy-done = s32[256,4096]{1,0:T(8,128)S(1)} copy-done((s32[256,4096]{1,0:T(8,128)S(1)}, s32[256,4096]{1,0:T(8,128)}, u32[]{:S(2)}) %copy-start) | copy-done | bytes 4194328
  2.9 1.6 %copy-done.1 = bf16[256,4096]{1,0:T(8,128)(2,1)S(1)} copy-done((bf16[256,4096]{1,0:T(8,128)(2,1)S(1)}, bf16[256,4096]{1,0:T(8,128)(2,1)}, u32[]{:S(2)}) %copy-start.1) | copy-done | bytes 2097176
  4.5 1.6 %copy-done.2 = bf16[256,4096]{1,0:T(8,128)(2,1)S(1)} copy-done((bf16[256,4096]{1,0:T(8,128)(2,1)S(1)}, bf16[256,4096]{1,0:T(8,128)(2,1)}, u32[]{:S(2)}) %copy-start.2) | copy-done | bytes 2097176
  6.1 2.0 %decode_key_value_1.1 = (bf16[256,1024]{1,0:T(8,128)(2,1)S(1)}, bf16[256,1024]{1,0:T(8,128)(2,1)S(1)}, bf16[256,1024]{1,0:T(8,128)(2,1)S(1)}, bf16[256,1024]{1,0:T(8,128)(2,1)S(1)}) custom-call(s32[4]{0:T(128)S(1)} %pad_add_fusion.place_ref, s32[256,4096]{1,0:T(8,128)S(1)} %copy-done, s32[256,4096]{1,0:T(8,128)S(1)} %copy-done, ...), custom_call_target="tpu_custom_call" | custom-call | flops 4194304 | bytes 6291456 | tf_op jit(solution)/shard_map/decode_key_value_1/pallas_call | solution.py:87
  8.1 0.5 collective-permute-start.11
  8.6 0.1 collective-permute-start.12
  8.7 2.0 %decode_key_value_0.1 = (bf16[256,1024]{1,0:T(8,128)(2,1)S(1)}, bf16[256,1024]{1,0:T(8,128)(2,1)S(1)}, bf16[256,1024]{1,0:T(8,128)(2,1)S(1)}, bf16[256,1024]{1,0:T(8,128)(2,1)S(1)}) custom-call(s32[4]{0:T(128)S(1)} %pad_add_fusion.place_ref, s32[256,4096]{1,0:T(8,128)S(1)} %copy-done, s32[256,4096]{1,0:T(8,128)S(1)} %copy-done, ...), custom_call_target="tpu_custom_call" | custom-call | flops 4194304 | bytes 6291456 | tf_op jit(solution)/shard_map/decode_key_value_0/pallas_call | solution.py:87
  10.7 0.5 collective-permute-start.1
  11.2 0.1 collective-permute-start.2
  11.3 1.7 %decode_query_1.1 = (bf16[256,1024]{1,0:T(8,128)(2,1)S(1)}, bf16[256,1024]{1,0:T(8,128)(2,1)S(1)}) custom-call(s32[4]{0:T(128)S(1)} %pad_add_fusion.place_ref, s32[256,4096]{1,0:T(8,128)S(1)} %copy-done, s32[256,4096]{1,0:T(8,128)S(1)} %copy-done, bf16[256,4096]{1,0:T(8,128)(2,1)S(1)} %copy-done.3, bf16[256,4096]{1,0:T(8,128)(2,1)S(1)} %copy-done.3), custom_call_target="tpu_custom_call" | custom-call | flops 4194304 | bytes 4194304 | tf_op jit(solution)/shard_map/decode_query_1/pallas_call | solution.py:87
  13.1 0.5 collective-permute-start.10
  13.5 1.7 %decode_query_0.1 = (bf16[256,1024]{1,0:T(8,128)(2,1)S(1)}, bf16[256,1024]{1,0:T(8,128)(2,1)S(1)}) custom-call(s32[4]{0:T(128)S(1)} %pad_add_fusion.place_ref, s32[256,4096]{1,0:T(8,128)S(1)} %copy-done, s32[256,4096]{1,0:T(8,128)S(1)} %copy-done, bf16[256,4096]{1,0:T(8,128)(2,1)S(1)} %copy-done.3, bf16[256,4096]{1,0:T(8,128)(2,1)S(1)} %copy-done.3), custom_call_target="tpu_custom_call" | custom-call | flops 4194304 | bytes 4194304 | tf_op jit(solution)/shard_map/decode_query_0/pallas_call | solution.py:87
  15.3 0.0 collective-permute-done.11.k_sib_ref
  15.3 0.2 collective-permute-start
  15.4 0.0 collective-permute-done.12.v_sib_ref
  15.5 1.4 %chunk_states.3 = (f32[2,128,128]{2,1,0:T(8,128)S(1)}, f32[4,2,128,128]{3,2,1,0:T(8,128)S(1)}, s16[272,128]{1,0:T(8,128)(2,1)S(1)}, s16[272,128]{1,0:T(8,128)(2,1)S(1)}, s16[272,128]{1,0:T(8,128)(2,1)S(1)}) custom-call(s32[4]{0:T(128)S(1)} %pad_add_fusion.place_ref, bf16[256,1024]{1,0:T(8,128)(2,1)S(1)} %get-tuple-element.51.k_ref, ...), custom_call_target="tpu_custom_call" | custom-call | flops 134217728 | bytes 2883584 | tf_op jit(solution)/shard_map/chunk_states/pallas_call | solution.py:169
  16.9 0.0 copy-start.4
  16.9 3.0 %collective-permute-start.13 = (s16[272,128]{1,0:T(8,128)(2,1)S(1)}, s16[272,128]{1,0:T(8,128)(2,1)S(1)}, u32[]{:S(2)}, u32[]{:S(2)}) collective-permute-start(s16[272,128]{1,0:T(8,128)(2,1)S(1)} %get-tuple-element.57), channel_id=1, source_target_pairs={{0,2},{2,0},{4,6},{6,4},{1,3},{3,1},{5,7},{7,5},{8,10},{10,8},{12,... | collective-permute-start | bytes 208904 | tf_op jit(solution)/shard_map/ppermute | solution.py:353
  19.9 0.0 collective-permute-done.1.k_sib_ref
  19.9 1.5 %collective-permute-start.14 = (s16[272,128]{1,0:T(8,128)(2,1)S(1)}, s16[272,128]{1,0:T(8,128)(2,1)S(1)}, u32[]{:S(2)}, u32[]{:S(2)}) collective-permute-start(s16[272,128]{1,0:T(8,128)(2,1)S(1)} %get-tuple-element.58), channel_id=1, source_target_pairs={{0,4},{2,6},{4,0},{6,2},{1,5},{3,7},{5,1},{7,3},{8,12},{10,14},{12... | collective-permute-start | bytes 208904 | tf_op jit(solution)/shard_map/ppermute | solution.py:353
  21.4 0.0 collective-permute-done.2.v_sib_ref
  21.4 0.1 collective-permute-start.15
  21.4 1.4 %chunk_states.2 = (f32[2,128,128]{2,1,0:T(8,128)S(1)}, f32[4,2,128,128]{3,2,1,0:T(8,128)S(1)}, s16[272,128]{1,0:T(8,128)(2,1)S(1)}, s16[272,128]{1,0:T(8,128)(2,1)S(1)}, s16[272,128]{1,0:T(8,128)(2,1)S(1)}) custom-call(s32[4]{0:T(128)S(1)} %pad_add_fusion.place_ref, bf16[256,1024]{1,0:T(8,128)(2,1)S(1)} %get-tuple-element.38.k_ref, ...), custom_call_target="tpu_custom_call" | custom-call | flops 134217728 | bytes 2883584 | tf_op jit(solution)/shard_map/chunk_states/pallas_call | solution.py:169
  22.9 0.0 collective-permute-done.13.refs_0_
  22.9 2.0 %collective-permute-start.3 = (s16[272,128]{1,0:T(8,128)(2,1)S(1)}, s16[272,128]{1,0:T(8,128)(2,1)S(1)}, u32[]{:S(2)}, u32[]{:S(2)}) collective-permute-start(s16[272,128]{1,0:T(8,128)(2,1)S(1)} %get-tuple-element.44), channel_id=1, source_target_pairs={{0,2},{2,0},{4,6},{6,4},{1,3},{3,1},{5,7},{7,5},{8,10},{10,8},{12,... | collective-permute-start | bytes 208904 | tf_op jit(solution)/shard_map/ppermute | solution.py:353
  24.9 0.1 collective-permute-done.14.refs_1_
  24.9 1.4 %collective-permute-start.4 = (s16[272,128]{1,0:T(8,128)(2,1)S(1)}, s16[272,128]{1,0:T(8,128)(2,1)S(1)}, u32[]{:S(2)}, u32[]{:S(2)}) collective-permute-start(s16[272,128]{1,0:T(8,128)(2,1)S(1)} %get-tuple-element.45), channel_id=1, source_target_pairs={{0,4},{2,6},{4,0},{6,2},{1,5},{3,7},{5,1},{7,3},{8,12},{10,14},{12... | collective-permute-start | bytes 208904 | tf_op jit(solution)/shard_map/ppermute | solution.py:353
  26.4 0.6 collective-permute-done.15.refs_2_
  27.0 0.6 collective-permute-start.5
  27.7 0.1 level_states.3
  27.8 0.0 collective-permute-done.3.refs_0_
  27.8 5.5 %collective-permute-start.18 = (s16[272,128]{1,0:T(8,128)(2,1)S(1)}, s16[272,128]{1,0:T(8,128)(2,1)S(1)}, u32[]{:S(2)}, u32[]{:S(2)}) collective-permute-start(s16[272,128]{1,0:T(8,128)(2,1)S(1)} %level_states.3), channel_id=1, source_target_pairs={{0,24},{1,25},{2,26},{3,27},{4,28},{5,29},{6,30},{7,31}} | collective-permute-start | bytes 208904 | tf_op jit(solution)/shard_map/ppermute | solution.py:360
  33.3 1.3 %collective-permute-start.17 = (s16[272,128]{1,0:T(8,128)(2,1)S(1)}, s16[272,128]{1,0:T(8,128)(2,1)S(1)}, u32[]{:S(2)}, u32[]{:S(2)}) collective-permute-start(s16[272,128]{1,0:T(8,128)(2,1)S(1)} %level_states.3), channel_id=1, source_target_pairs={{0,16},{8,24},{1,17},{9,25},{2,18},{10,26},{3,19},{11,27},{4,20},{... | collective-permute-start | bytes 208904 | tf_op jit(solution)/shard_map/ppermute | solution.py:360
  34.6 0.0 collective-permute-done.5.refs_2_
  34.6 3.1 %collective-permute-start.16 = (s16[272,128]{1,0:T(8,128)(2,1)S(1)}, s16[272,128]{1,0:T(8,128)(2,1)S(1)}, u32[]{:S(2)}, u32[]{:S(2)}) collective-permute-start(s16[272,128]{1,0:T(8,128)(2,1)S(1)} %level_states.3), channel_id=1, source_target_pairs={{0,8},{8,16},{16,24},{1,9},{9,17},{17,25},{2,10},{10,18},{18,26},{... | collective-permute-start | bytes 208904 | tf_op jit(solution)/shard_map/ppermute | solution.py:360
  37.7 0.1 level_states.2
  37.9 3.5 %collective-permute-start.8 = (s16[272,128]{1,0:T(8,128)(2,1)S(1)}, s16[272,128]{1,0:T(8,128)(2,1)S(1)}, u32[]{:S(2)}, u32[]{:S(2)}) collective-permute-start(s16[272,128]{1,0:T(8,128)(2,1)S(1)} %level_states.2), channel_id=1, source_target_pairs={{0,24},{1,25},{2,26},{3,27},{4,28},{5,29},{6,30},{7,31}} | collective-permute-start | bytes 208904 | tf_op jit(solution)/shard_map/ppermute | solution.py:360
  41.4 1.3 %collective-permute-start.7 = (s16[272,128]{1,0:T(8,128)(2,1)S(1)}, s16[272,128]{1,0:T(8,128)(2,1)S(1)}, u32[]{:S(2)}, u32[]{:S(2)}) collective-permute-start(s16[272,128]{1,0:T(8,128)(2,1)S(1)} %level_states.2), channel_id=1, source_target_pairs={{0,16},{8,24},{1,17},{9,25},{2,18},{10,26},{3,19},{11,27},{4,20},{... | collective-permute-start | bytes 208904 | tf_op jit(solution)/shard_map/ppermute | solution.py:360
  42.7 3.0 %collective-permute-start.6 = (s16[272,128]{1,0:T(8,128)(2,1)S(1)}, s16[272,128]{1,0:T(8,128)(2,1)S(1)}, u32[]{:S(2)}, u32[]{:S(2)}) collective-permute-start(s16[272,128]{1,0:T(8,128)(2,1)S(1)} %level_states.2), channel_id=1, source_target_pairs={{0,8},{8,16},{16,24},{1,9},{9,17},{17,25},{2,10},{10,18},{18,26},{... | collective-permute-start | bytes 208904 | tf_op jit(solution)/shard_map/ppermute | solution.py:360
  45.8 0.9 %carries.3 = (s16[272,128]{1,0:T(8,128)(2,1)S(1)}, s16[272,128]{1,0:T(8,128)(2,1)S(1)}, s16[272,128]{1,0:T(8,128)(2,1)S(1)}, s16[272,128]{1,0:T(8,128)(2,1)S(1)}...) custom-call(s32[4]{0:T(128)S(1)} %pad_add_fusion.place_ref, f32[2,128,128]{2,1,0:T(8,128)S(1)} %get-tuple-element.56.own_ref, ...), custom_call_target="tpu_custom_call" | custom-call | bytes 1245184 | tf_op jit(solution)/shard_map/carries/pallas_call | solution.py:234
  46.7 1.6 %collective-permute-start.24 = (s16[272,128]{1,0:T(8,128)(2,1)S(1)}, s16[272,128]{1,0:T(8,128)(2,1)S(1)}, u32[]{:S(2)}, u32[]{:S(2)}) collective-permute-start(s16[272,128]{1,0:T(8,128)(2,1)S(1)} %get-tuple-element.64), channel_id=1, source_target_pairs={{0,2},{2,0},{4,6},{6,4},{1,3},{3,1},{5,7},{7,5},{8,10},{10,8},{12,... | collective-permute-start | bytes 208904 | tf_op jit(solution)/shard_map/ppermute | solution.py:353
  48.4 1.8 %collective-permute-start.25 = (s16[272,128]{1,0:T(8,128)(2,1)S(1)}, s16[272,128]{1,0:T(8,128)(2,1)S(1)}, u32[]{:S(2)}, u32[]{:S(2)}) collective-permute-start(s16[272,128]{1,0:T(8,128)(2,1)S(1)} %get-tuple-element.65), channel_id=1, source_target_pairs={{0,6},{2,4},{4,2},{6,0},{1,7},{3,5},{5,3},{7,1},{8,14},{10,12},{12... | collective-permute-start | bytes 208904 | tf_op jit(solution)/shard_map/ppermute | solution.py:353
  50.1 1.9 %collective-permute-start.20 = (f32[1,1024]{1,0:T(1,128)S(1)}, f32[1,1024]{1,0:T(1,128)S(1)}, u32[]{:S(2)}, u32[]{:S(2)}) collective-permute-start(f32[1,1024]{1,0:T(1,128)S(1)} %bitcast.5), channel_id=1, source_target_pairs={{0,2},{2,0},{1,3},{3,1},{4,6},{6,4},{5,7},{7,5},{8,10},{10,8},{9,1... | collective-permute-start | bytes 12296 | tf_op jit(solution)/shard_map/ppermute | solution.py:353
  52.1 0.9 %carries.2 = (s16[272,128]{1,0:T(8,128)(2,1)S(1)}, s16[272,128]{1,0:T(8,128)(2,1)S(1)}, s16[272,128]{1,0:T(8,128)(2,1)S(1)}, s16[272,128]{1,0:T(8,128)(2,1)S(1)}...) custom-call(s32[4]{0:T(128)S(1)} %pad_add_fusion.place_ref, f32[2,128,128]{2,1,0:T(8,128)S(1)} %get-tuple-element.43.own_ref, ...), custom_call_target="tpu_custom_call" | custom-call | bytes 1245184 | tf_op jit(solution)/shard_map/carries/pallas_call | solution.py:234
  53.0 0.7 collective-permute-done.20.gain_ref
  53.7 1.9 %collective-permute-start.21 = (s16[272,128]{1,0:T(8,128)(2,1)S(1)}, s16[272,128]{1,0:T(8,128)(2,1)S(1)}, u32[]{:S(2)}, u32[]{:S(2)}) collective-permute-start(s16[272,128]{1,0:T(8,128)(2,1)S(1)} %get-tuple-element.62), channel_id=1, source_target_pairs={{0,2},{2,0},{4,6},{6,4},{1,3},{3,1},{5,7},{7,5},{8,10},{10,8},{12,... | collective-permute-start | bytes 208904 | tf_op jit(solution)/shard_map/ppermute | solution.py:353
  55.7 0.1 collective-permute-start.22
  55.8 1.9 %attend_1_1.1 = bf16[512,512]{1,0:T(8,128)(2,1)S(1)} custom-call(s32[4]{0:T(128)S(1)} %pad_add_fusion.place_ref, bf16[256,1024]{1,0:T(8,128)(2,1)S(1)} %get-tuple-element.49.q_ref, bf16[256,1024]{1,0:T(8,128)(2,1)S(1)} %collective-permute-done.10.q_sib_ref, bf16[256,1024]{1,0:T(8,128)(2,1)S(1)} %get-tuple-element.51.k_ref, ...), custom_call_target="tpu_custom_call" | custom-call | flops 402653184 | bytes 2097152 | tf_op jit(solution)/shard_map/attend_1_1/pallas_call | solution.py:292
  57.7 1.8 %collective-permute-start.26 = (bf16[512,512]{1,0:T(8,128)(2,1)S(1)}, bf16[512,512]{1,0:T(8,128)(2,1)S(1)}, u32[]{:S(2)}, u32[]{:S(2)}) collective-permute-start(bf16[512,512]{1,0:T(8,128)(2,1)S(1)} %attend_1_1.1), channel_id=1, source_target_pairs={{0,2},{2,0},{1,3},{3,1},{4,6},{6,4},{5,7},{7,5},{8,10},{10,8},{9,1... | collective-permute-start | bytes 1572872 | tf_op jit(solution)/shard_map/ppermute | solution.py:353
  59.5 2.1 %collective-permute-done.22.refs_1_ = s16[272,128]{1,0:T(8,128)(2,1)S(1)} collective-permute-done((s16[272,128]{1,0:T(8,128)(2,1)S(1)}, s16[272,128]{1,0:T(8,128)(2,1)S(1)}, u32[]{:S(2)}, u32[]{:S(2)}) %collective-permute-start.22) | collective-permute-done | bytes 69664 | tf_op jit(solution)/shard_map/ppermute | solution.py:353
  61.6 1.9 %attend_0_1.1 = bf16[512,512]{1,0:T(8,128)(2,1)S(1)} custom-call(s32[4]{0:T(128)S(1)} %pad_add_fusion.place_ref, bf16[256,1024]{1,0:T(8,128)(2,1)S(1)} %get-tuple-element.36.q_ref, bf16[256,1024]{1,0:T(8,128)(2,1)S(1)} %collective-permute-done.q_sib_ref, bf16[256,1024]{1,0:T(8,128)(2,1)S(1)} %get-tuple-element.38.k_ref, ...), custom_call_target="tpu_custom_call" | custom-call | flops 402653184 | bytes 2097152 | tf_op jit(solution)/shard_map/attend_0_1/pallas_call | solution.py:292
  63.5 0.1 collective-permute-start.23
  63.6 0.5 collective-permute-start.19
  64.0 1.6 %collective-permute-start.28 = (f32[2,128,128]{2,1,0:T(8,128)S(1)}, f32[2,128,128]{2,1,0:T(8,128)S(1)}, u32[]{:S(2)}, u32[]{:S(2)}) collective-permute-start(f32[2,128,128]{2,1,0:T(8,128)S(1)} %get-tuple-element.69), channel_id=1, source_target_pairs={{0,4},{4,0},{1,5},{5,1},{2,6},{6,2},{3,7},{7,3},{8,12},{12,8},{9,1... | collective-permute-start | bytes 393224 | tf_op jit(solution)/shard_map/ppermute | solution.py:353
  65.7 0.4 collective-permute-start.27
  66.1 1.9 %collective-permute-done.19.refs_1_ = s16[272,128]{1,0:T(8,128)(2,1)S(1)} collective-permute-done((s16[272,128]{1,0:T(8,128)(2,1)S(1)}, s16[272,128]{1,0:T(8,128)(2,1)S(1)}, u32[]{:S(2)}, u32[]{:S(2)}) %collective-permute-start.19) | collective-permute-done | bytes 69664 | tf_op jit(solution)/shard_map/ppermute | solution.py:353
  68.0 0.4 collective-permute-start.9
  68.4 1.9 %attend_1_0.1.refs_1_ = bf16[512,512]{1,0:T(8,128)(2,1)S(1)} custom-call(s32[4]{0:T(128)S(1)} %pad_add_fusion.place_ref, bf16[256,1024]{1,0:T(8,128)(2,1)S(1)} %get-tuple-element.49.q_ref, bf16[256,1024]{1,0:T(8,128)(2,1)S(1)} %collective-permute-done.10.q_sib_ref, bf16[256,1024]{1,0:T(8,128)(2,1)S(1)} %get-tuple-element.51.k_ref, ...), custom_call_target="tpu_custom_call" | custom-call | flops 402653184 | bytes 2097152 | tf_op jit(solution)/shard_map/attend_1_0/pallas_call | solution.py:292
  70.2 2.0 %collective-permute-done.9.refs_1_ = s16[272,128]{1,0:T(8,128)(2,1)S(1)} collective-permute-done((s16[272,128]{1,0:T(8,128)(2,1)S(1)}, s16[272,128]{1,0:T(8,128)(2,1)S(1)}, u32[]{:S(2)}, u32[]{:S(2)}) %collective-permute-start.9) | collective-permute-done | bytes 69664 | tf_op jit(solution)/shard_map/ppermute | solution.py:353
  72.3 1.9 %attend_0_0.1.refs_0_ = bf16[512,512]{1,0:T(8,128)(2,1)S(1)} custom-call(s32[4]{0:T(128)S(1)} %pad_add_fusion.place_ref, bf16[256,1024]{1,0:T(8,128)(2,1)S(1)} %get-tuple-element.36.q_ref, bf16[256,1024]{1,0:T(8,128)(2,1)S(1)} %collective-permute-done.q_sib_ref, bf16[256,1024]{1,0:T(8,128)(2,1)S(1)} %get-tuple-element.38.k_ref, ...), custom_call_target="tpu_custom_call" | custom-call | flops 402653184 | bytes 2097152 | tf_op jit(solution)/shard_map/attend_0_0/pallas_call | solution.py:292
  74.2 1.4 %assemble_cache.1 = f32[1,8,128,128]{3,2,1,0:T(8,128)} custom-call(s32[4]{0:T(128)S(1)} %pad_add_fusion.place_ref, f32[2,128,128]{2,1,0:T(8,128)S(1)} %get-tuple-element.66.refs_0_, f32[2,128,128]{2,1,0:T(8,128)S(1)} %collective-permute-done.27.refs_1_, f32[2,128,128]{2,1,0:T(8,128)S(1)} %get-tuple-element.68.refs_2_, ...), custom_call_target="tpu_custom_call" | custom-call | tf_op jit(solution)/shard_map/assemble_cache/pallas_call | solution.py:338
  75.6 2.4 %collective-permute-done.23.refs_2_ = bf16[512,512]{1,0:T(8,128)(2,1)S(1)} collective-permute-done((bf16[512,512]{1,0:T(8,128)(2,1)S(1)}, bf16[512,512]{1,0:T(8,128)(2,1)S(1)}, u32[]{:S(2)}, u32[]{:S(2)}) %collective-permute-start.23) | collective-permute-done | bytes 524320 | tf_op jit(solution)/shard_map/ppermute | solution.py:353
  78.0 2.0 %assemble.1 = bf16[1024,1024]{1,0:T(8,128)(2,1)} custom-call(s32[4]{0:T(128)S(1)} %pad_add_fusion.place_ref, bf16[512,512]{1,0:T(8,128)(2,1)S(1)} %attend_0_0.1.refs_0_, bf16[512,512]{1,0:T(8,128)(2,1)S(1)} %attend_1_0.1.refs_1_, bf16[512,512]{1,0:T(8,128)(2,1)S(1)} %collective-permute-done.23.refs_2_, bf16[512,512]{1,0:T(8,128)(2,1)S(1)} %collective-permute-done.26.refs_3_), custom_call_target="tpu_custom_call" | custom-call | tf_op jit(solution)/shard_map/assemble/pallas_call | solution.py:317
  (21 shorter events, 0.0 us)
Async XLA Ops:
  0.7 2.2 %copy-start = (s32[256,4096]{1,0:T(8,128)S(1)}, s32[256,4096]{1,0:T(8,128)}, u32[]{:S(2)}) copy-start(s32[256,4096]{1,0:T(8,128)} %refs_1_.7) | copy-start | bytes 12582916
  2.9 1.6 %copy-start.1 = (bf16[256,4096]{1,0:T(8,128)(2,1)S(1)}, bf16[256,4096]{1,0:T(8,128)(2,1)}, u32[]{:S(2)}) copy-start(bf16[256,4096]{1,0:T(8,128)(2,1)} %refs_3_.7) | copy-start | bytes 6291460
  4.5 1.6 %copy-start.2 = (bf16[256,4096]{1,0:T(8,128)(2,1)S(1)}, bf16[256,4096]{1,0:T(8,128)(2,1)}, u32[]{:S(2)}) copy-start(bf16[256,4096]{1,0:T(8,128)(2,1)} %refs_5_.3) | copy-start | bytes 6291460
  8.1 7.2 %collective-permute-start.11 = (bf16[256,1024]{1,0:T(8,128)(2,1)S(1)}, bf16[256,1024]{1,0:T(8,128)(2,1)S(1)}, u32[]{:S(2)}, u32[]{:S(2)}) collective-permute-start(bf16[256,1024]{1,0:T(8,128)(2,1)S(1)} %get-tuple-element.52), channel_id=1, source_target_pairs={{0,1},{1,0},{2,3},{3,2},{4,5},{5,4},{6,7},{7,6},{8,9},{9,8},{10,11... | collective-permute-start | bytes 1572872 | tf_op jit(solution)/shard_map/ppermute | solution.py:353
  8.6 2.7 %copy-start.3 = (bf16[256,4096]{1,0:T(8,128)(2,1)S(1)}, bf16[256,4096]{1,0:T(8,128)(2,1)}, u32[]{:S(2)}) copy-start(bf16[256,4096]{1,0:T(8,128)(2,1)} %refs_3_.6) | copy-start | bytes 6291460
  8.6 6.8 %collective-permute-start.12 = (bf16[256,1024]{1,0:T(8,128)(2,1)S(1)}, bf16[256,1024]{1,0:T(8,128)(2,1)S(1)}, u32[]{:S(2)}, u32[]{:S(2)}) collective-permute-start(bf16[256,1024]{1,0:T(8,128)(2,1)S(1)} %get-tuple-element.54), channel_id=1, source_target_pairs={{0,1},{1,0},{2,3},{3,2},{4,5},{5,4},{6,7},{7,6},{8,9},{9,8},{10,11... | collective-permute-start | bytes 1572872 | tf_op jit(solution)/shard_map/ppermute | solution.py:353
  10.7 9.1 %collective-permute-start.1 = (bf16[256,1024]{1,0:T(8,128)(2,1)S(1)}, bf16[256,1024]{1,0:T(8,128)(2,1)S(1)}, u32[]{:S(2)}, u32[]{:S(2)}) collective-permute-start(bf16[256,1024]{1,0:T(8,128)(2,1)S(1)} %get-tuple-element.39), channel_id=1, source_target_pairs={{0,1},{1,0},{2,3},{3,2},{4,5},{5,4},{6,7},{7,6},{8,9},{9,8},{10,11... | collective-permute-start | bytes 1572872 | tf_op jit(solution)/shard_map/ppermute | solution.py:353
  11.2 10.1 %collective-permute-start.2 = (bf16[256,1024]{1,0:T(8,128)(2,1)S(1)}, bf16[256,1024]{1,0:T(8,128)(2,1)S(1)}, u32[]{:S(2)}, u32[]{:S(2)}) collective-permute-start(bf16[256,1024]{1,0:T(8,128)(2,1)S(1)} %get-tuple-element.41), channel_id=1, source_target_pairs={{0,1},{1,0},{2,3},{3,2},{4,5},{5,4},{6,7},{7,6},{8,9},{9,8},{10,11... | collective-permute-start | bytes 1572872 | tf_op jit(solution)/shard_map/ppermute | solution.py:353
  13.1 42.6 %collective-permute-start.10 = (bf16[256,1024]{1,0:T(8,128)(2,1)S(1)}, bf16[256,1024]{1,0:T(8,128)(2,1)S(1)}, u32[]{:S(2)}, u32[]{:S(2)}) collective-permute-start(bf16[256,1024]{1,0:T(8,128)(2,1)S(1)} %get-tuple-element.50), channel_id=1, source_target_pairs={{0,1},{1,0},{2,3},{3,2},{4,5},{5,4},{6,7},{7,6},{8,9},{9,8},{10,11... | collective-permute-start | bytes 1572872 | tf_op jit(solution)/shard_map/ppermute | solution.py:353
  15.3 44.2 %collective-permute-start = (bf16[256,1024]{1,0:T(8,128)(2,1)S(1)}, bf16[256,1024]{1,0:T(8,128)(2,1)S(1)}, u32[]{:S(2)}, u32[]{:S(2)}) collective-permute-start(bf16[256,1024]{1,0:T(8,128)(2,1)S(1)} %get-tuple-element.37), channel_id=1, source_target_pairs={{0,1},{1,0},{2,3},{3,2},{4,5},{5,4},{6,7},{7,6},{8,9},{9,8},{10,11... | collective-permute-start | bytes 1572872 | tf_op jit(solution)/shard_map/ppermute | solution.py:353
  16.9 33.2 %copy-start.4 = (f32[1024]{0:T(1024)S(1)}, f32[1024]{0:T(1024)}, u32[]{:S(2)}) copy-start(f32[1024]{0:T(1024)} %param.9) | copy-start | bytes 12292
  16.9 6.0 %collective-permute-start.13 = (s16[272,128]{1,0:T(8,128)(2,1)S(1)}, s16[272,128]{1,0:T(8,128)(2,1)S(1)}, u32[]{:S(2)}, u32[]{:S(2)}) collective-permute-start(s16[272,128]{1,0:T(8,128)(2,1)S(1)} %get-tuple-element.57), channel_id=1, source_target_pairs={{0,2},{2,0},{4,6},{6,4},{1,3},{3,1},{5,7},{7,5},{8,10},{10,8},{12,... | collective-permute-start | bytes 208904 | tf_op jit(solution)/shard_map/ppermute | solution.py:353
  19.9 5.1 %collective-permute-start.14 = (s16[272,128]{1,0:T(8,128)(2,1)S(1)}, s16[272,128]{1,0:T(8,128)(2,1)S(1)}, u32[]{:S(2)}, u32[]{:S(2)}) collective-permute-start(s16[272,128]{1,0:T(8,128)(2,1)S(1)} %get-tuple-element.58), channel_id=1, source_target_pairs={{0,4},{2,6},{4,0},{6,2},{1,5},{3,7},{5,1},{7,3},{8,12},{10,14},{12... | collective-permute-start | bytes 208904 | tf_op jit(solution)/shard_map/ppermute | solution.py:353
  21.4 5.6 %collective-permute-start.15 = (s16[272,128]{1,0:T(8,128)(2,1)S(1)}, s16[272,128]{1,0:T(8,128)(2,1)S(1)}, u32[]{:S(2)}, u32[]{:S(2)}) collective-permute-start(s16[272,128]{1,0:T(8,128)(2,1)S(1)} %get-tuple-element.59), channel_id=1, source_target_pairs={{0,6},{2,4},{4,2},{6,0},{1,7},{3,5},{5,3},{7,1},{8,14},{10,12},{12... | collective-permute-start | bytes 208904 | tf_op jit(solution)/shard_map/ppermute | solution.py:353
  22.9 4.9 %collective-permute-start.3 = (s16[272,128]{1,0:T(8,128)(2,1)S(1)}, s16[272,128]{1,0:T(8,128)(2,1)S(1)}, u32[]{:S(2)}, u32[]{:S(2)}) collective-permute-start(s16[272,128]{1,0:T(8,128)(2,1)S(1)} %get-tuple-element.44), channel_id=1, source_target_pairs={{0,2},{2,0},{4,6},{6,4},{1,3},{3,1},{5,7},{7,5},{8,10},{10,8},{12,... | collective-permute-start | bytes 208904 | tf_op jit(solution)/shard_map/ppermute | solution.py:353
  24.9 8.4 %collective-permute-start.4 = (s16[272,128]{1,0:T(8,128)(2,1)S(1)}, s16[272,128]{1,0:T(8,128)(2,1)S(1)}, u32[]{:S(2)}, u32[]{:S(2)}) collective-permute-start(s16[272,128]{1,0:T(8,128)(2,1)S(1)} %get-tuple-element.45), channel_id=1, source_target_pairs={{0,4},{2,6},{4,0},{6,2},{1,5},{3,7},{5,1},{7,3},{8,12},{10,14},{12... | collective-permute-start | bytes 208904 | tf_op jit(solution)/shard_map/ppermute | solution.py:353
  27.0 7.6 %collective-permute-start.5 = (s16[272,128]{1,0:T(8,128)(2,1)S(1)}, s16[272,128]{1,0:T(8,128)(2,1)S(1)}, u32[]{:S(2)}, u32[]{:S(2)}) collective-permute-start(s16[272,128]{1,0:T(8,128)(2,1)S(1)} %get-tuple-element.46), channel_id=1, source_target_pairs={{0,6},{2,4},{4,2},{6,0},{1,7},{3,5},{5,3},{7,1},{8,14},{10,12},{12... | collective-permute-start | bytes 208904 | tf_op jit(solution)/shard_map/ppermute | solution.py:353
  27.8 10.1 %collective-permute-start.18 = (s16[272,128]{1,0:T(8,128)(2,1)S(1)}, s16[272,128]{1,0:T(8,128)(2,1)S(1)}, u32[]{:S(2)}, u32[]{:S(2)}) collective-permute-start(s16[272,128]{1,0:T(8,128)(2,1)S(1)} %level_states.3), channel_id=1, source_target_pairs={{0,24},{1,25},{2,26},{3,27},{4,28},{5,29},{6,30},{7,31}} | collective-permute-start | bytes 208904 | tf_op jit(solution)/shard_map/ppermute | solution.py:360
  33.3 8.1 %collective-permute-start.17 = (s16[272,128]{1,0:T(8,128)(2,1)S(1)}, s16[272,128]{1,0:T(8,128)(2,1)S(1)}, u32[]{:S(2)}, u32[]{:S(2)}) collective-permute-start(s16[272,128]{1,0:T(8,128)(2,1)S(1)} %level_states.3), channel_id=1, source_target_pairs={{0,16},{8,24},{1,17},{9,25},{2,18},{10,26},{3,19},{11,27},{4,20},{... | collective-permute-start | bytes 208904 | tf_op jit(solution)/shard_map/ppermute | solution.py:360
  34.6 8.1 %collective-permute-start.16 = (s16[272,128]{1,0:T(8,128)(2,1)S(1)}, s16[272,128]{1,0:T(8,128)(2,1)S(1)}, u32[]{:S(2)}, u32[]{:S(2)}) collective-permute-start(s16[272,128]{1,0:T(8,128)(2,1)S(1)} %level_states.3), channel_id=1, source_target_pairs={{0,8},{8,16},{16,24},{1,9},{9,17},{17,25},{2,10},{10,18},{18,26},{... | collective-permute-start | bytes 208904 | tf_op jit(solution)/shard_map/ppermute | solution.py:360
  37.9 8.9 %collective-permute-start.8 = (s16[272,128]{1,0:T(8,128)(2,1)S(1)}, s16[272,128]{1,0:T(8,128)(2,1)S(1)}, u32[]{:S(2)}, u32[]{:S(2)}) collective-permute-start(s16[272,128]{1,0:T(8,128)(2,1)S(1)} %level_states.2), channel_id=1, source_target_pairs={{0,24},{1,25},{2,26},{3,27},{4,28},{5,29},{6,30},{7,31}} | collective-permute-start | bytes 208904 | tf_op jit(solution)/shard_map/ppermute | solution.py:360
  41.4 6.9 %collective-permute-start.7 = (s16[272,128]{1,0:T(8,128)(2,1)S(1)}, s16[272,128]{1,0:T(8,128)(2,1)S(1)}, u32[]{:S(2)}, u32[]{:S(2)}) collective-permute-start(s16[272,128]{1,0:T(8,128)(2,1)S(1)} %level_states.2), channel_id=1, source_target_pairs={{0,16},{8,24},{1,17},{9,25},{2,18},{10,26},{3,19},{11,27},{4,20},{... | collective-permute-start | bytes 208904 | tf_op jit(solution)/shard_map/ppermute | solution.py:360
  42.7 7.4 %collective-permute-start.6 = (s16[272,128]{1,0:T(8,128)(2,1)S(1)}, s16[272,128]{1,0:T(8,128)(2,1)S(1)}, u32[]{:S(2)}, u32[]{:S(2)}) collective-permute-start(s16[272,128]{1,0:T(8,128)(2,1)S(1)} %level_states.2), channel_id=1, source_target_pairs={{0,8},{8,16},{16,24},{1,9},{9,17},{17,25},{2,10},{10,18},{18,26},{... | collective-permute-start | bytes 208904 | tf_op jit(solution)/shard_map/ppermute | solution.py:360
  46.7 9.1 %collective-permute-start.24 = (s16[272,128]{1,0:T(8,128)(2,1)S(1)}, s16[272,128]{1,0:T(8,128)(2,1)S(1)}, u32[]{:S(2)}, u32[]{:S(2)}) collective-permute-start(s16[272,128]{1,0:T(8,128)(2,1)S(1)} %get-tuple-element.64), channel_id=1, source_target_pairs={{0,2},{2,0},{4,6},{6,4},{1,3},{3,1},{5,7},{7,5},{8,10},{10,8},{12,... | collective-permute-start | bytes 208904 | tf_op jit(solution)/shard_map/ppermute | solution.py:353
  48.4 7.4 %collective-permute-start.25 = (s16[272,128]{1,0:T(8,128)(2,1)S(1)}, s16[272,128]{1,0:T(8,128)(2,1)S(1)}, u32[]{:S(2)}, u32[]{:S(2)}) collective-permute-start(s16[272,128]{1,0:T(8,128)(2,1)S(1)} %get-tuple-element.65), channel_id=1, source_target_pairs={{0,6},{2,4},{4,2},{6,0},{1,7},{3,5},{5,3},{7,1},{8,14},{10,12},{12... | collective-permute-start | bytes 208904 | tf_op jit(solution)/shard_map/ppermute | solution.py:353
  50.1 3.6 %collective-permute-start.20 = (f32[1,1024]{1,0:T(1,128)S(1)}, f32[1,1024]{1,0:T(1,128)S(1)}, u32[]{:S(2)}, u32[]{:S(2)}) collective-permute-start(f32[1,1024]{1,0:T(1,128)S(1)} %bitcast.5), channel_id=1, source_target_pairs={{0,2},{2,0},{1,3},{3,1},{4,6},{6,4},{5,7},{7,5},{8,10},{10,8},{9,1... | collective-permute-start | bytes 12296 | tf_op jit(solution)/shard_map/ppermute | solution.py:353
  53.7 5.8 %collective-permute-start.21 = (s16[272,128]{1,0:T(8,128)(2,1)S(1)}, s16[272,128]{1,0:T(8,128)(2,1)S(1)}, u32[]{:S(2)}, u32[]{:S(2)}) collective-permute-start(s16[272,128]{1,0:T(8,128)(2,1)S(1)} %get-tuple-element.62), channel_id=1, source_target_pairs={{0,2},{2,0},{4,6},{6,4},{1,3},{3,1},{5,7},{7,5},{8,10},{10,8},{12,... | collective-permute-start | bytes 208904 | tf_op jit(solution)/shard_map/ppermute | solution.py:353
  55.7 6.0 %collective-permute-start.22 = (s16[272,128]{1,0:T(8,128)(2,1)S(1)}, s16[272,128]{1,0:T(8,128)(2,1)S(1)}, u32[]{:S(2)}, u32[]{:S(2)}) collective-permute-start(s16[272,128]{1,0:T(8,128)(2,1)S(1)} %get-tuple-element.63), channel_id=1, source_target_pairs={{0,6},{2,4},{4,2},{6,0},{1,7},{3,5},{5,3},{7,1},{8,14},{10,12},{12... | collective-permute-start | bytes 208904 | tf_op jit(solution)/shard_map/ppermute | solution.py:353
  57.7 17.9 %collective-permute-start.26 = (bf16[512,512]{1,0:T(8,128)(2,1)S(1)}, bf16[512,512]{1,0:T(8,128)(2,1)S(1)}, u32[]{:S(2)}, u32[]{:S(2)}) collective-permute-start(bf16[512,512]{1,0:T(8,128)(2,1)S(1)} %attend_1_1.1), channel_id=1, source_target_pairs={{0,2},{2,0},{1,3},{3,1},{4,6},{6,4},{5,7},{7,5},{8,10},{10,8},{9,1... | collective-permute-start | bytes 1572872 | tf_op jit(solution)/shard_map/ppermute | solution.py:353
  63.5 14.5 %collective-permute-start.23 = (bf16[512,512]{1,0:T(8,128)(2,1)S(1)}, bf16[512,512]{1,0:T(8,128)(2,1)S(1)}, u32[]{:S(2)}, u32[]{:S(2)}) collective-permute-start(bf16[512,512]{1,0:T(8,128)(2,1)S(1)} %attend_0_1.1), channel_id=1, source_target_pairs={{0,2},{2,0},{1,3},{3,1},{4,6},{6,4},{5,7},{7,5},{8,10},{10,8},{9,1... | collective-permute-start | bytes 1572872 | tf_op jit(solution)/shard_map/ppermute | solution.py:353
  63.6 4.4 %collective-permute-start.19 = (s16[272,128]{1,0:T(8,128)(2,1)S(1)}, s16[272,128]{1,0:T(8,128)(2,1)S(1)}, u32[]{:S(2)}, u32[]{:S(2)}) collective-permute-start(s16[272,128]{1,0:T(8,128)(2,1)S(1)} %get-tuple-element.61), channel_id=1, source_target_pairs={{0,4},{2,6},{4,0},{6,2},{1,5},{3,7},{5,1},{7,3},{8,12},{10,14},{12... | collective-permute-start | bytes 208904 | tf_op jit(solution)/shard_map/ppermute | solution.py:353
  64.0 10.1 %collective-permute-start.28 = (f32[2,128,128]{2,1,0:T(8,128)S(1)}, f32[2,128,128]{2,1,0:T(8,128)S(1)}, u32[]{:S(2)}, u32[]{:S(2)}) collective-permute-start(f32[2,128,128]{2,1,0:T(8,128)S(1)} %get-tuple-element.69), channel_id=1, source_target_pairs={{0,4},{4,0},{1,5},{5,1},{2,6},{6,2},{3,7},{7,3},{8,12},{12,8},{9,1... | collective-permute-start | bytes 393224 | tf_op jit(solution)/shard_map/ppermute | solution.py:353
  65.7 8.5 %collective-permute-start.27 = (f32[2,128,128]{2,1,0:T(8,128)S(1)}, f32[2,128,128]{2,1,0:T(8,128)S(1)}, u32[]{:S(2)}, u32[]{:S(2)}) collective-permute-start(f32[2,128,128]{2,1,0:T(8,128)S(1)} %get-tuple-element.67), channel_id=1, source_target_pairs={{0,4},{4,0},{1,5},{5,1},{2,6},{6,2},{3,7},{7,3},{8,12},{12,8},{9,1... | collective-permute-start | bytes 393224 | tf_op jit(solution)/shard_map/ppermute | solution.py:353
  68.0 4.3 %collective-permute-start.9 = (s16[272,128]{1,0:T(8,128)(2,1)S(1)}, s16[272,128]{1,0:T(8,128)(2,1)S(1)}, u32[]{:S(2)}, u32[]{:S(2)}) collective-permute-start(s16[272,128]{1,0:T(8,128)(2,1)S(1)} %get-tuple-element.48), channel_id=1, source_target_pairs={{0,4},{2,6},{4,0},{6,2},{1,5},{3,7},{5,1},{7,3},{8,12},{10,14},{12... | collective-permute-start | bytes 208904 | tf_op jit(solution)/shard_map/ppermute | solution.py:353

commit v3 on v2

v3 whole, which is shorter than its diff:
```python
import functools

import jax
import jax.numpy as jnp
from jax import lax
from jax.experimental import pallas as pl
from jax.experimental.pallas import tpu as pltpu
from jax.sharding import Mesh
from jax.sharding import PartitionSpec as P

HD = 128
SCORE_SCALE = HD ** (-0.5)
CORES = 2
VMEM_BYTES = 24 * 1024 * 1024
DECODE_VMEM_BYTES = 52 * 1024 * 1024
PAD = 16
TOP = 32767.0

VMEM = pl.BlockSpec(memory_space=pltpu.VMEM)
SMEM = pl.BlockSpec(memory_space=pltpu.SMEM)
HBM = pl.BlockSpec(memory_space=pltpu.HBM)
ANY = pl.BlockSpec(memory_space=pl.ANY)


def params(n_axes=0, vmem=VMEM_BYTES):
    return pltpu.CompilerParams(
        dimension_semantics=("arbitrary",) * n_axes or None, vmem_limit_bytes=vmem
    )


def cost(flops, bytes_accessed):
    return pl.CostEstimate(flops=flops, bytes_accessed=bytes_accessed, transcendentals=0)


class Plan:
    def __init__(self, mesh, rows, model):
        n_seq, n_head = mesh.shape["seq"], mesh.shape["head"]
        self.n_y = n_head // CORES
        self.width = model // n_head
        group = self.width // HD
        self.n_inner = 2 if n_seq % 2 == 0 and group % 2 == 0 else 1
        self.n_outer = n_seq // self.n_inner
        self.halves = 2 if group // self.n_inner % 2 == 0 else 1
        self.each = group // (self.n_inner * self.halves)
        self.plane = self.n_inner * self.n_y
        self.rows = rows
        self.block = rows * n_head
        self.owned = self.halves * self.each
        self.piece = self.each * HD


def counts_of(spikes, names):
    one, two = jnp.ones_like(spikes), jnp.full_like(spikes, 2)
    zero = jnp.zeros_like(spikes)

    def ternary(rest, unit):
        return jnp.where(rest >= 2 * unit, two, jnp.where(rest >= unit, one, zero))

    counts = {"value": ternary(spikes, 9)}
    if names != ("value",):
        rest = spikes - 9 * counts["value"]
        counts["key"] = ternary(rest, 3)
        if "query" in names:
            counts["query"] = rest - 3 * counts["key"]
    return counts


def decode(plan, place, spikes, operands, after=()):
    names = tuple(operands)
    rows, model = spikes.shape
    step = min(rows, 64)
    width = plan.width
    n = len(names)

    def kernel(place_ref, spikes_ref, *refs):
        outs = refs[n + len(after) :]
        for side in range(CORES):
            of = place_ref[0] if side == 0 else 1 - place_ref[0]
            at = pl.ds(pl.multiple_of(of * width, width), width)
            spikes = spikes_ref[:, at].astype(jnp.float32).astype(jnp.bfloat16)
            counts = counts_of(spikes, names)
            for index, name in enumerate(names):
                outs[2 * index + side][...] = refs[index][:, at] * counts[name]

    return pl.pallas_call(
        kernel,
        out_shape=[jax.ShapeDtypeStruct((rows, plan.n_y * width), jnp.bfloat16)] * (2 * n),
        grid_spec=pltpu.PrefetchScalarGridSpec(
            num_scalar_prefetch=1,
            grid=(rows // step, plan.n_y),
            in_specs=[pl.BlockSpec((step, CORES * width), lambda r, y, place: (r, y))] * (1 + n)
            + [ANY] * len(after),
            out_specs=[pl.BlockSpec((step, width), lambda r, y, place: (r, y))] * (2 * n),
        ),
        compiler_params=params(2, DECODE_VMEM_BYTES),
        cost_estimate=cost(rows * model * 4, rows * model * (4 + 4 * n)),
        name="decode_" + "_".join(names),
    )(place, spikes, *operands.values(), *after)


def contract_rows(left, right):
    return lax.dot_general(
        left, right, (((0,), (0,)), ((), ())), preferred_element_type=jnp.float32
    )


def contract_columns(left, right):
    return lax.dot_general(
        left, right, (((1,), (1,)), ((), ())), preferred_element_type=jnp.float32
    )


def code(states, ref):
    line = lax.broadcasted_iota(jnp.int32, (PAD, HD), 0)
    exponents = jnp.zeros((PAD, HD), jnp.float32)
    for i, state in enumerate(states):
        top = jnp.max(jnp.abs(state), axis=0, keepdims=True)
        exponent = jnp.floor(jnp.log2(jnp.maximum(top, 1e-30))) + 1
        scaled = jnp.round(state * jnp.exp2(15 - exponent))
        scaled = jnp.clip(scaled, -TOP, TOP)
        ref[i * HD : (i + 1) * HD] = scaled.astype(jnp.int32).astype(jnp.int16)
        exponents = jnp.where(line == i, exponent, exponents)
    ref[len(states) * HD :] = exponents.astype(jnp.int32).astype(jnp.int16)


def decoded(ref, which=None):
    count = ref.shape[0] // HD
    exponents = ref[count * HD :].astype(jnp.int32).astype(jnp.float32)
    return [
        ref[i * HD : (i + 1) * HD].astype(jnp.int32).astype(jnp.float32)
        * jnp.exp2(exponents[i : i + 1] - 15)
        for i in (range(count) if which is None else which)
    ]


def plus(left, right):
    return [a + b for a, b in zip(left, right)]


def coded_shape(heads):
    return jax.ShapeDtypeStruct((heads * HD + PAD, HD), jnp.int16)


def states_shape(*lead):
    return jax.ShapeDtypeStruct((*lead, HD, HD), jnp.float32)


def owned_columns(plan, place_ref, offset, half, i):
    x = place_ref[1] ^ (offset // plan.n_y)
    y = place_ref[2] ^ (offset % plan.n_y)
    start = (((y * plan.halves + half) * plan.n_inner + x) * plan.each + i) * HD
    return pl.ds(pl.multiple_of(start, HD), HD)


def chunk_states(plan, place, key, value, after):
    def kernel(place_ref, k_ref, k_sib_ref, v_ref, v_sib_ref, *refs):
        own_ref, first_ref, *send_refs = refs[len(after) :]
        is_first = jnp.full((HD, HD), place_ref[0], jnp.int32) == 0
        for offset in (*range(1, plan.plane), 0):
            states = []
            for half in range(plan.halves):
                for i in range(plan.each):
                    at = owned_columns(plan, place_ref, offset, half, i)
                    mine = contract_rows(v_ref[:, at], k_ref[:, at])
                    sib = contract_rows(v_sib_ref[:, at], k_sib_ref[:, at])
                    first_ref[offset, half * plan.each + i] = jnp.where(is_first, mine, sib)
                    states.append(mine + sib)
            if offset:
                code(states, send_refs[offset - 1])
            else:
                for i, state in enumerate(states):
                    own_ref[i] = state

    heads = plan.plane * plan.owned
    return pl.pallas_call(
        kernel,
        out_shape=[states_shape(plan.owned), states_shape(plan.plane, plan.owned)]
        + [coded_shape(plan.owned)] * (plan.plane - 1),
        in_specs=[SMEM] + [VMEM] * 4 + [ANY] * len(after),
        out_specs=[VMEM] * (1 + plan.plane),
        compiler_params=params(),
        cost_estimate=cost(
            4 * plan.rows * HD * HD * heads, 8 * plan.rows * HD * heads + 6 * heads * HD * HD
        ),
        name="chunk_states",
    )(place, *key, *value, *after)


def of_half(plan, half):
    return range(half * plan.each, (half + 1) * plan.each)


def level_states(plan, own, others, half):
    def kernel(own_ref, *refs):
        *other_refs, total_ref, coded_ref = refs
        total = [own_ref[i] for i in of_half(plan, half)]
        for ref in other_refs:
            total = plus(total, decoded(ref, of_half(plan, half)))
        for i, state in enumerate(total):
            total_ref[i] = state
        code(total, coded_ref)

    return pl.pallas_call(
        kernel,
        out_shape=[states_shape(plan.each), coded_shape(plan.each)],
        in_specs=[VMEM] * plan.plane,
        out_specs=[VMEM] * 2,
        compiler_params=params(),
        cost_estimate=cost(0, plan.plane * plan.each * HD * HD * 2),
        name=f"level_states_{half}",
    )(own, *others)


def levels_so_far(plan, total, arrived, half):
    def kernel(total_ref, *refs):
        total = [total_ref[i] for i in range(plan.each)]
        for ref in refs[:-1]:
            total = plus(total, decoded(ref))
        code(total, refs[-1])

    return pl.pallas_call(
        kernel,
        out_shape=coded_shape(plan.each),
        in_specs=[VMEM] * (1 + len(arrived)),
        out_specs=VMEM,
        compiler_params=params(),
        cost_estimate=cost(0, 2 * plan.each * HD * HD * 2),
        name=f"levels_so_far_{half}_{len(arrived)}",
    )(total, *arrived)


def carries(plan, place, own, others, levels, half, after=()):
    n_others, n_levels = len(others), len(levels)
    heads = of_half(plan, half)

    def kernel(place_ref, own_ref, *refs):
        other_refs = refs[:n_others]
        level_refs = refs[n_others : n_others + n_levels]
        outs = refs[n_others + n_levels + len(after) :]
        x, y, level = place_ref[1], place_ref[2], place_ref[3]
        here = x * plan.n_y + y
        earlier = [jnp.zeros((HD, HD), jnp.float32)] * plan.each
        for ref in level_refs:
            earlier = plus(earlier, decoded(ref))
        states = [[own_ref[i] for i in heads]]
        states += [decoded(ref, heads) for ref in other_refs]

        def add(totals, keep_of):
            for offset, terms in enumerate(states):
                keep = jnp.full((HD, HD), keep_of(here ^ offset), jnp.int32) == 1
                totals = plus(totals, [jnp.where(keep, s, 0.0) for s in terms])
            return totals

        for offset, ref in enumerate(outs[: plan.plane]):
            to = here ^ offset
            code(add(earlier, lambda chip: (chip < to).astype(jnp.int32)), ref)
        for offset, ref in enumerate(outs[plan.plane :]):
            to = x ^ offset
            block = level * plan.n_inner + to
            seen = jnp.full((1, HD), (block + 1) * plan.block, jnp.int32).astype(jnp.float32)
            totals = add(earlier, lambda chip: (chip // plan.n_y <= to).astype(jnp.int32))
            for i, total in enumerate(totals):
                ref[i] = total.T * lax.rsqrt(seen)

    return pl.pallas_call(
        kernel,
        out_shape=[coded_shape(plan.each)] * plan.plane + [states_shape(plan.each)] * plan.n_inner,
        in_specs=[SMEM] + [VMEM] * (1 + n_others + n_levels) + [ANY] * len(after),
        out_specs=[VMEM] * (plan.plane + plan.n_inner),
        compiler_params=params(),
        cost_estimate=cost(0, (plan.plane * 4 + n_levels) * plan.each * HD * HD * 2),
        name=f"carries_{half}",
    )(place, own, *others, *levels, *after)


def attend(plan, place, query, key, value, carry, first, gain, half, offsets):
    rows = plan.rows

    def kernel(
        place_ref, q_ref, q_sib_ref, k_ref, k_sib_ref, v_ref, v_sib_ref, first_ref, gain_ref, *refs
    ):
        core = place_ref[0]
        out_ref = refs[-1]
        causal = lax.broadcasted_iota(jnp.int32, (rows, rows), 0) >= lax.broadcasted_iota(
            jnp.int32, (rows, rows), 1
        )
        is_second = jnp.full((HD, HD), core, jnp.int32) == 1

        def attended(q_ref, k_ref, v_ref, at, carried, gain):
            queries = q_ref[:, at]
            scores = contract_columns(queries, k_ref[:, at]) * SCORE_SCALE
            weights = jnp.where(causal, scores, 0.0).astype(jnp.bfloat16)
            raw = jnp.dot(weights, v_ref[:, at], preferred_element_type=jnp.float32)
            carried = carried * SCORE_SCALE
            high = carried.astype(jnp.bfloat16)
            low = (carried - high.astype(jnp.float32)).astype(jnp.bfloat16)
            both = contract_columns(queries, jnp.concatenate([high, low], axis=0))
            raw = raw + (both[:, :HD] + both[:, HD:])
            mean = jnp.mean(raw * raw, axis=-1, keepdims=True)
            return (raw * lax.rsqrt(mean + 1e-06) * gain).astype(jnp.bfloat16)

        for piece, offset in enumerate(offsets):
            x = place_ref[1] ^ (offset // plan.n_y)
            carry_states = decoded(refs[piece])
            for i in range(plan.each):
                at = owned_columns(plan, place_ref, offset, half, i)
                start = ((half * plan.n_inner + x) * plan.each + i) * HD
                gain = gain_ref[:, pl.ds(pl.multiple_of(start, HD), HD)]
                out_at = slice(piece * plan.piece + i * HD, piece * plan.piece + (i + 1) * HD)
                first = first_ref[offset, half * plan.each + i]
                mine = carry_states[i] + jnp.where(is_second, first, 0.0)
                sib = carry_states[i] + jnp.where(is_second, 0.0, first)
                out_ref[pl.ds(pl.multiple_of(core * rows, rows), rows), out_at] = attended(
                    q_ref, k_ref, v_ref, at, mine, gain
                )
                out_ref[pl.ds(pl.multiple_of((1 - core) * rows, rows), rows), out_at] = attended(
                    q_sib_ref, k_sib_ref, v_sib_ref, at, sib, gain
                )

    heads = len(offsets) * plan.each
    return pl.pallas_call(
        kernel,
        out_shape=jax.ShapeDtypeStruct((CORES * rows, heads * HD), jnp.bfloat16),
        in_specs=[SMEM] + [VMEM] * (8 + len(offsets)),
        out_specs=VMEM,
        compiler_params=params(),
        cost_estimate=cost(
            heads * (8 * rows * rows * HD + 8 * rows * HD * HD), 16 * rows * heads * HD
        ),
        name=f"attend_{half}_" + "_".join(map(str, offsets)),
    )(place, *query, *key, *value, first, gain, *carry)


def assemble(plan, place, parts, into=None):
    rows = CORES * plan.rows
    copies = [(n, piece, half, o) for n, (_, half, os) in enumerate(parts) for piece, o in enumerate(os)]

    def kernel(place_ref, *refs):
        out_ref, sems = refs[-2:]
        started = []
        for at, (n, piece, half, offset) in enumerate(copies):
            x = place_ref[1] ^ (offset // plan.n_y)
            y = place_ref[2] ^ (offset % plan.n_y)
            column = (half * plan.n_inner + x) * plan.piece
            to_rows = pl.ds(pl.multiple_of(y * rows, rows), rows)
            to_columns = pl.ds(pl.multiple_of(column, plan.piece), plan.piece)
            started.append(
                pltpu.make_async_copy(
                    refs[n].at[:, pl.ds(piece * plan.piece, plan.piece)],
                    out_ref.at[to_rows, to_columns],
                    sems.at[at],
                )
            )
            started[-1].start()
        for copy in started:
            copy.wait()

    arrays = [array for array, _, _ in parts]
    aliased = [] if into is None else [into]
    return pl.pallas_call(
        kernel,
        out_shape=jax.ShapeDtypeStruct((plan.n_y * rows, plan.width), jnp.bfloat16),
        in_specs=[SMEM] + [VMEM] * len(arrays) + [HBM] * len(aliased),
        out_specs=HBM,
        scratch_shapes=[pltpu.SemaphoreType.DMA((len(copies),))],
        input_output_aliases={1 + len(arrays): 0} if aliased else {},
        compiler_params=params(),
        name="assemble" if into is None else "finish",
    )(place, *arrays, *aliased)


def assemble_cache(plan, place, parts):
    heads = plan.halves * plan.n_inner * plan.each

    def kernel(place_ref, *refs):
        out_ref = refs[-1]
        for half in range(plan.halves):
            for offset_x in range(plan.n_inner):
                x = place_ref[1] ^ offset_x
                start = (half * plan.n_inner + x) * plan.each
                out_ref[0, pl.ds(start, plan.each)] = refs[half * plan.n_inner + offset_x][...]

    return pl.pallas_call(
        kernel,
        out_shape=jax.ShapeDtypeStruct((1, heads, HD, HD), jnp.float32),
        in_specs=[SMEM] + [VMEM] * (plan.halves * plan.n_inner),
        out_specs=VMEM,
        compiler_params=params(),
        name="assemble_cache",
    )(place, *[part for offsets in parts for part in offsets])


def per_device(plan, queries, keys, values, spikes, gain):
    place = jnp.stack([lax.axis_index(a) for a in ("core", "inner", "y", "outer")]).astype(jnp.int32)
    halves = range(plan.halves)

    def swap(array, axes, offset, size):
        return lax.ppermute(array, axes, [(i, i ^ offset) for i in range(size)])

    def in_level(array, offset):
        return swap(array, ("inner", "y"), offset, plan.plane)

    def to_later(array, distance):
        pairs = [(i, i + distance) for i in range(plan.n_outer - distance)]
        return lax.ppermute(array, "outer", pairs)

    def spiked(operands, after=()):
        arrays = decode(plan, place, spikes, operands, after)
        return [
            (arrays[2 * i], swap(arrays[2 * i + 1], "core", 1, CORES)) for i in range(len(operands))
        ]

    gain = gain.reshape(1, plan.width)
    gains = [gain] + [swap(gain, "y", o, plan.n_y) for o in range(1, plan.n_y)]
    key, value = spiked({"key": keys, "value": values})
    own, first, *sends = chunk_states(plan, place, key, value, gains[1:])
    others = [in_level(a, o) for o, a in enumerate(sends, 1)]
    (query,) = spiked({"query": queries}, (own,))

    totals = [level_states(plan, own, others, half) for half in halves]
    sums = [coded for _, coded in totals]
    arrived = [[] for _ in halves]
    distance = 1
    while distance < plan.n_outer:
        for half in halves:
            arrived[half].append(to_later(sums[half], distance))
        distance *= 2
        if distance < plan.n_outer:
            sums = [levels_so_far(plan, totals[half][0], arrived[half], half) for half in halves]

    parts, caches = [], []
    carry = [None] * plan.halves
    of_group = [list(range(y, plan.plane, plan.n_y)) for y in range(plan.n_y)]

    def part_of(half, offsets):
        return attend(
            plan,
            place,
            query,
            key,
            value,
            [carry[half][o] for o in offsets],
            first,
            gains[offsets[0] % plan.n_y],
            half,
            offsets,
        )

    for half in halves:
        outs = carries(plan, place, own, others, arrived[half], half)
        mine, *sends = outs[: plan.plane]
        carry[half] = [mine] + [in_level(a, o) for o, a in enumerate(sends, 1)]
        cache, *sends = outs[plan.plane :]
        caches.append([cache] + [swap(a, "inner", o, plan.n_inner) for o, a in enumerate(sends, 1)])
    for half in halves:
        for y in range(1, plan.n_y):
            for offsets in [[o] for o in of_group[y]] if half == 0 else [of_group[y]]:
                part = part_of(half, offsets)
                parts.append((swap(part, "y", y, plan.n_y), half, offsets))
    early = [(part_of(half, of_group[0]), half, of_group[0]) for half in halves]
    out = assemble(plan, place, early + parts[:-1])
    out = assemble(plan, place, parts[-1:], out)
    return out, assemble_cache(plan, place, caches)


def solution(mesh):
    tokens = P(("outer", "inner", "y", "core"), None)
    seq, head = ("outer", "inner"), ("y", "core")

    def whole(queries, keys, values, spikes, gain):
        plan = Plan(mesh, spikes.shape[0] // mesh.size, spikes.shape[1])
        sizes = (plan.n_outer, plan.n_inner, plan.n_y, CORES)
        split = Mesh(mesh.devices.reshape(sizes), ("outer", "inner", "y", "core"))
        return jax.shard_map(
            functools.partial(per_device, plan),
            mesh=split,
            in_specs=(tokens, tokens, tokens, tokens, P(head)),
            out_specs=(P(seq, head), P(seq, head, None, None)),
            check_vma=False,
        )(queries, keys, values, spikes, gain)

    return whole
```

time: 80.3 us -> 99.5 us (1.24)
  waiting for transfers between devices: 9.96 us -> 24.3 us
  Pallas kernels: 23.3 us -> 32.3 us
  local copies, waits for them, and re-layouts: 5.38 us -> 1.23 us
    pallas_call x4 -> x2, Pallas kernels: 7.49 us -> 15.3 us  [decode(): pl.pallas_call(kernel, out_shape=[jax.ShapeDtypeStruct((rows, plan.n_y *...]
    ppermute x6 -> x4, waiting for transfers between devices: 0.02 us -> 7.69 us  [to_later(): return lax.ppermute(array, 'outer', pairs)]
    ppermute x23 -> x18, waiting for transfers between devices: 9.95 us -> 16.6 us  [swap(): return lax.ppermute(array, axes, [(i, i ^ offset) for i in range(size)])]
    unnamed x10 -> x6, local copies, waits for them, and re-layouts: 5.38 us -> 1.23 us
    ppermute x23 -> x18, starting transfers between devices: 22.6 us -> 20.7 us  [swap(): return lax.ppermute(array, axes, [(i, i ^ offset) for i in range(size)])]
    ppermute x6 -> x4, starting transfers between devices: 17.8 us -> 19.3 us  [to_later(): return lax.ppermute(array, 'outer', pairs)]
    pallas_call x1 -> x2, Pallas kernels: 2.02 us -> 3.09 us  [assemble(): pl.pallas_call(kernel, out_shape=jax.ShapeDtypeStruct((plan.n_y * rows, p...]
    pallas_call x10 -> x12, Pallas kernels: 12.4 us -> 12.6 us  [the longest x5 8.29 us: attend(): pl.pallas_call(kernel, out_shape=jax.ShapeDtypeStruct((CORES * rows, head...]
  transfers between devices with their start and end apart: 29 -> 22, of which waited for: 7 -> 12; matrix products, arithmetic and copies ran while one was open for 0% -> 0% of each run, Pallas kernels for 24% -> 12%
where the time goes in v3:
time: 99.5 us; the launch traced here: 98.8 us
  starting transfers between devices  40.1 us (40%)
  Pallas kernels  32.3 us (32%)
  waiting for transfers between devices  24.3 us (24%)
  local copies, waits for them, and re-layouts  1.23 us (1%)
    ppermute x18, starting transfers between devices, swap(): return lax.ppermute(array, axes, [(i, i ^ offset) for i in range(size)])  20.7 us
    ppermute x4, starting transfers between devices, to_later(): return lax.ppermute(array, 'outer', pairs)  19.3 us
    ppermute x18, waiting for transfers between devices, swap(): return lax.ppermute(array, axes, [(i, i ^ offset) for i in range(size)])  16.6 us
    pallas_call x2, Pallas kernels, decode(): pl.pallas_call(kernel, out_shape=[jax.ShapeDtypeStruct((rows, plan.n_y *...  15.3 us
    pallas_call x5, Pallas kernels, attend(): pl.pallas_call(kernel, out_shape=jax.ShapeDtypeStruct((CORES * rows, head...  8.29 us
    ppermute x4, waiting for transfers between devices, to_later(): return lax.ppermute(array, 'outer', pairs)  7.69 us
    pallas_call x2, Pallas kernels, assemble(): pl.pallas_call(kernel, out_shape=jax.ShapeDtypeStruct((plan.n_y * rows, p...  3.09 us
    pallas_call x1, Pallas kernels, chunk_states(): pl.pallas_call(kernel, out_shape=[states_shape(plan.owned), states_shape(...  2.11 us
  transfers between devices with their start and end apart: 22, of which 12 were waited for; matrix products, arithmetic and copies ran while one was open for 0% of the time, Pallas kernels for 12%

profile of v3, /device:TPU:0, one launch (start us, length us, event | category | flops | bytes accessed | tf_op | source)
XLA Modules:
  0.0 98.8 jit_solution(13601210290582066895)
XLA Ops:
  0.6 0.1 pad_add_fusion.place_ref
  0.7 8.1 %decode_key_value.1 = (bf16[256,2048]{1,0:T(8,128)(2,1)S(1)}, bf16[256,2048]{1,0:T(8,128)(2,1)}, bf16[256,2048]{1,0:T(8,128)(2,1)}, bf16[256,2048]{1,0:T(8,128)(2,1)}) custom-call(s32[4]{0:T(128)S(1)} %pad_add_fusion.place_ref, s32[256,4096]{1,0:T(8,128)} %spikes_ref.3, bf16[256,4096]{1,0:T(8,128)(2,1)} %refs_0_.2, bf16[256,4096]{1,0:T(8,128)(2,1)} %refs_1_.1), custom_call_target="tpu_custom_call" | custom-call | flops 4194304 | bytes 12582912 | tf_op jit(solution)/shard_map/decode_key_value/pallas_call | solution.py:85
  8.8 0.5 collective-permute-start
  9.2 0.1 collective-permute-start.1
  9.3 0.0 copy-done.2
  9.3 3.0 %collective-permute-start.2 = (f32[1,1024]{1,0:T(1,128)S(1)}, f32[1,1024]{1,0:T(1,128)S(1)}, u32[]{:S(2)}, u32[]{:S(2)}) collective-permute-start(f32[1,1024]{1,0:T(1,128)S(1)} %bitcast.5), channel_id=1, source_target_pairs={{0,2},{2,0},{1,3},{3,1},{4,6},{6,4},{5,7},{7,5},{8,10},{10,8},{9,1... | collective-permute-start | bytes 12296 | tf_op jit(solution)/shard_map/ppermute | solution.py:398
  12.3 1.6 %collective-permute-done.2.refs_0_.gain_ref = f32[1,1024]{1,0:T(1,128)S(1)} collective-permute-done((f32[1,1024]{1,0:T(1,128)S(1)}, f32[1,1024]{1,0:T(1,128)S(1)}, u32[]{:S(2)}, u32[]{:S(2)}) %collective-permute-start.2) | collective-permute-done | bytes 4128 | tf_op jit(solution)/shard_map/ppermute | solution.py:398
  13.9 0.0 collective-permute-done.k_sib_ref
  13.9 0.0 collective-permute-done.1.v_sib_ref
  13.9 1.2 %copy-done = bf16[256,2048]{1,0:T(8,128)(2,1)S(1)} copy-done((bf16[256,2048]{1,0:T(8,128)(2,1)S(1)}, bf16[256,2048]{1,0:T(8,128)(2,1)}, u32[]{:S(2)}) %copy-start) | copy-done | bytes 1048600
  15.1 2.1 %chunk_states.1 = (f32[4,128,128]{2,1,0:T(8,128)S(1)}, f32[4,4,128,128]{3,2,1,0:T(8,128)S(1)}, s16[528,128]{1,0:T(8,128)(2,1)S(1)}, s16[528,128]{1,0:T(8,128)(2,1)S(1)}, s16[528,128]{1,0:T(8,128)(2,1)S(1)}) custom-call(s32[4]{0:T(128)S(1)} %pad_add_fusion.place_ref, bf16[256,2048]{1,0:T(8,128)(2,1)S(1)} %get-tuple-element.29.k_ref, ...), custom_call_target="tpu_custom_call" | custom-call | flops 268435456 | bytes 5767168 | tf_op jit(solution)/shard_map/chunk_states/pallas_call | solution.py:175
  17.2 7.2 %decode_query.1 = (bf16[256,2048]{1,0:T(8,128)(2,1)S(1)}, bf16[256,2048]{1,0:T(8,128)(2,1)}) custom-call(s32[4]{0:T(128)S(1)} %pad_add_fusion.place_ref, s32[256,4096]{1,0:T(8,128)} %spikes_ref.3, bf16[256,4096]{1,0:T(8,128)(2,1)} %refs_0_.3, f32[4,128,128]{2,1,0:T(8,128)S(1)} %get-tuple-element.33.refs_1_.own_ref), custom_call_target="tpu_custom_call" | custom-call | flops 4194304 | bytes 8388608 | tf_op jit(solution)/shard_map/decode_query/pallas_call | solution.py:85
  24.4 0.0 collective-permute-start.3
  24.4 2.4 %collective-permute-start.4 = (s16[528,128]{1,0:T(8,128)(2,1)S(1)}, s16[528,128]{1,0:T(8,128)(2,1)S(1)}, u32[]{:S(2)}, u32[]{:S(2)}) collective-permute-start(s16[528,128]{1,0:T(8,128)(2,1)S(1)} %get-tuple-element.37), channel_id=1, source_target_pairs={{0,2},{2,0},{4,6},{6,4},{1,3},{3,1},{5,7},{7,5},{8,10},{10,8},{12,... | collective-permute-start | bytes 405512 | tf_op jit(solution)/shard_map/ppermute | solution.py:398
  26.8 1.5 %collective-permute-start.5 = (s16[528,128]{1,0:T(8,128)(2,1)S(1)}, s16[528,128]{1,0:T(8,128)(2,1)S(1)}, u32[]{:S(2)}, u32[]{:S(2)}) collective-permute-start(s16[528,128]{1,0:T(8,128)(2,1)S(1)} %get-tuple-element.38), channel_id=1, source_target_pairs={{0,4},{2,6},{4,0},{6,2},{1,5},{3,7},{5,1},{7,3},{8,12},{10,14},{12... | collective-permute-start | bytes 405512 | tf_op jit(solution)/shard_map/ppermute | solution.py:398
  28.3 0.0 collective-permute-start.6
  28.3 2.6 %collective-permute-done.4.refs_0_ = s16[528,128]{1,0:T(8,128)(2,1)S(1)} collective-permute-done((s16[528,128]{1,0:T(8,128)(2,1)S(1)}, s16[528,128]{1,0:T(8,128)(2,1)S(1)}, u32[]{:S(2)}, u32[]{:S(2)}) %collective-permute-start.4) | collective-permute-done | bytes 135200 | tf_op jit(solution)/shard_map/ppermute | solution.py:398
  30.9 2.3 %collective-permute-done.5.refs_1_ = s16[528,128]{1,0:T(8,128)(2,1)S(1)} collective-permute-done((s16[528,128]{1,0:T(8,128)(2,1)S(1)}, s16[528,128]{1,0:T(8,128)(2,1)S(1)}, u32[]{:S(2)}, u32[]{:S(2)}) %collective-permute-start.5) | collective-permute-done | bytes 135200 | tf_op jit(solution)/shard_map/ppermute | solution.py:398
  33.3 1.7 %collective-permute-done.6.refs_2_ = s16[528,128]{1,0:T(8,128)(2,1)S(1)} collective-permute-done((s16[528,128]{1,0:T(8,128)(2,1)S(1)}, s16[528,128]{1,0:T(8,128)(2,1)S(1)}, u32[]{:S(2)}, u32[]{:S(2)}) %collective-permute-start.6) | collective-permute-done | bytes 135200 | tf_op jit(solution)/shard_map/ppermute | solution.py:398
  35.0 0.1 level_states_1.1
  35.1 3.7 %collective-permute-start.7 = (s16[272,128]{1,0:T(8,128)(2,1)S(1)}, s16[272,128]{1,0:T(8,128)(2,1)S(1)}, u32[]{:S(2)}, u32[]{:S(2)}) collective-permute-start(s16[272,128]{1,0:T(8,128)(2,1)S(1)} %get-tuple-element.40), channel_id=1, source_target_pairs={{0,8},{8,16},{16,24},{1,9},{9,17},{17,25},{2,10},{10,18},{18,26},{... | collective-permute-start | bytes 208904 | tf_op jit(solution)/shard_map/ppermute | solution.py:405
  38.8 1.9 %collective-permute-done.7.refs_0_.refs_3_ = s16[272,128]{1,0:T(8,128)(2,1)S(1)} collective-permute-done((s16[272,128]{1,0:T(8,128)(2,1)S(1)}, s16[272,128]{1,0:T(8,128)(2,1)S(1)}, u32[]{:S(2)}, u32[]{:S(2)}) %collective-permute-start.7) | collective-permute-done | bytes 69664 | tf_op jit(solution)/shard_map/ppermute | solution.py:405
  40.8 0.1 levels_so_far_1_1.1
  40.8 5.3 %collective-permute-start.8 = (s16[272,128]{1,0:T(8,128)(2,1)S(1)}, s16[272,128]{1,0:T(8,128)(2,1)S(1)}, u32[]{:S(2)}, u32[]{:S(2)}) collective-permute-start(s16[272,128]{1,0:T(8,128)(2,1)S(1)} %levels_so_far_1_1.1), channel_id=1, source_target_pairs={{0,16},{8,24},{1,17},{9,25},{2,18},{10,26},{3,19},{11,27},{4,20},{... | collective-permute-start | bytes 208904 | tf_op jit(solution)/shard_map/ppermute | solution.py:405
  46.1 1.9 %collective-permute-done.8.refs_4_ = s16[272,128]{1,0:T(8,128)(2,1)S(1)} collective-permute-done((s16[272,128]{1,0:T(8,128)(2,1)S(1)}, s16[272,128]{1,0:T(8,128)(2,1)S(1)}, u32[]{:S(2)}, u32[]{:S(2)}) %collective-permute-start.8) | collective-permute-done | bytes 69664 | tf_op jit(solution)/shard_map/ppermute | solution.py:405
  48.1 0.9 carries_1.1
  49.0 1.6 %collective-permute-start.9 = (s16[272,128]{1,0:T(8,128)(2,1)S(1)}, s16[272,128]{1,0:T(8,128)(2,1)S(1)}, u32[]{:S(2)}, u32[]{:S(2)}) collective-permute-start(s16[272,128]{1,0:T(8,128)(2,1)S(1)} %get-tuple-element.42), channel_id=1, source_target_pairs={{0,2},{2,0},{4,6},{6,4},{1,3},{3,1},{5,7},{7,5},{8,10},{10,8},{12,... | collective-permute-start | bytes 208904 | tf_op jit(solution)/shard_map/ppermute | solution.py:398
  50.6 1.4 %collective-permute-start.10 = (s16[272,128]{1,0:T(8,128)(2,1)S(1)}, s16[272,128]{1,0:T(8,128)(2,1)S(1)}, u32[]{:S(2)}, u32[]{:S(2)}) collective-permute-start(s16[272,128]{1,0:T(8,128)(2,1)S(1)} %get-tuple-element.43), channel_id=1, source_target_pairs={{0,6},{2,4},{4,2},{6,0},{1,7},{3,5},{5,3},{7,1},{8,14},{10,12},{12... | collective-permute-start | bytes 208904 | tf_op jit(solution)/shard_map/ppermute | solution.py:398
  52.0 1.3 %collective-permute-done.9.refs_0_ = s16[272,128]{1,0:T(8,128)(2,1)S(1)} collective-permute-done((s16[272,128]{1,0:T(8,128)(2,1)S(1)}, s16[272,128]{1,0:T(8,128)(2,1)S(1)}, u32[]{:S(2)}, u32[]{:S(2)}) %collective-permute-start.9) | collective-permute-done | bytes 69664 | tf_op jit(solution)/shard_map/ppermute | solution.py:398
  53.3 2.4 %collective-permute-done.10.refs_1_ = s16[272,128]{1,0:T(8,128)(2,1)S(1)} collective-permute-done((s16[272,128]{1,0:T(8,128)(2,1)S(1)}, s16[272,128]{1,0:T(8,128)(2,1)S(1)}, u32[]{:S(2)}, u32[]{:S(2)}) %collective-permute-start.10) | collective-permute-done | bytes 69664 | tf_op jit(solution)/shard_map/ppermute | solution.py:398
  55.8 0.0 collective-permute-done.3.q_sib_ref
  55.8 1.9 %attend_1_1_3.1 = bf16[512,512]{1,0:T(8,128)(2,1)S(1)} custom-call(s32[4]{0:T(128)S(1)} %pad_add_fusion.place_ref, bf16[256,2048]{1,0:T(8,128)(2,1)S(1)} %get-tuple-element.34.q_ref, bf16[256,2048]{1,0:T(8,128)(2,1)S(1)} %collective-permute-done.3.q_sib_ref, bf16[256,2048]{1,0:T(8,128)(2,1)S(1)} %get-tuple-element.29.k_ref, ...), custom_call_target="tpu_custom_call" | custom-call | flops 402653184 | bytes 2097152 | tf_op jit(solution)/shard_map/attend_1_1_3/pallas_call | solution.py:321
  57.6 0.6 collective-permute-start.11
  58.2 0.1 level_states_0.1
  58.3 4.0 %collective-permute-start.12 = (s16[272,128]{1,0:T(8,128)(2,1)S(1)}, s16[272,128]{1,0:T(8,128)(2,1)S(1)}, u32[]{:S(2)}, u32[]{:S(2)}) collective-permute-start(s16[272,128]{1,0:T(8,128)(2,1)S(1)} %get-tuple-element.44), channel_id=1, source_target_pairs={{0,8},{8,16},{16,24},{1,9},{9,17},{17,25},{2,10},{10,18},{18,26},{... | collective-permute-start | bytes 208904 | tf_op jit(solution)/shard_map/ppermute | solution.py:405
  62.3 1.9 %collective-permute-done.12.refs_0_.refs_3_ = s16[272,128]{1,0:T(8,128)(2,1)S(1)} collective-permute-done((s16[272,128]{1,0:T(8,128)(2,1)S(1)}, s16[272,128]{1,0:T(8,128)(2,1)S(1)}, u32[]{:S(2)}, u32[]{:S(2)}) %collective-permute-start.12) | collective-permute-done | bytes 69664 | tf_op jit(solution)/shard_map/ppermute | solution.py:405
  64.2 0.1 levels_so_far_0_1.1
  64.3 6.3 %collective-permute-start.13 = (s16[272,128]{1,0:T(8,128)(2,1)S(1)}, s16[272,128]{1,0:T(8,128)(2,1)S(1)}, u32[]{:S(2)}, u32[]{:S(2)}) collective-permute-start(s16[272,128]{1,0:T(8,128)(2,1)S(1)} %levels_so_far_0_1.1), channel_id=1, source_target_pairs={{0,16},{8,24},{1,17},{9,25},{2,18},{10,26},{3,19},{11,27},{4,20},{... | collective-permute-start | bytes 208904 | tf_op jit(solution)/shard_map/ppermute | solution.py:405
  70.7 1.9 %collective-permute-done.13.refs_4_ = s16[272,128]{1,0:T(8,128)(2,1)S(1)} collective-permute-done((s16[272,128]{1,0:T(8,128)(2,1)S(1)}, s16[272,128]{1,0:T(8,128)(2,1)S(1)}, u32[]{:S(2)}, u32[]{:S(2)}) %collective-permute-start.13) | collective-permute-done | bytes 69664 | tf_op jit(solution)/shard_map/ppermute | solution.py:405
  72.6 0.9 carries_0.1
  73.5 1.8 %collective-permute-start.16 = (s16[272,128]{1,0:T(8,128)(2,1)S(1)}, s16[272,128]{1,0:T(8,128)(2,1)S(1)}, u32[]{:S(2)}, u32[]{:S(2)}) collective-permute-start(s16[272,128]{1,0:T(8,128)(2,1)S(1)} %get-tuple-element.50), channel_id=1, source_target_pairs={{0,2},{2,0},{4,6},{6,4},{1,3},{3,1},{5,7},{7,5},{8,10},{10,8},{12,... | collective-permute-start | bytes 208904 | tf_op jit(solution)/shard_map/ppermute | solution.py:398
  75.3 1.5 %collective-permute-start.18 = (s16[272,128]{1,0:T(8,128)(2,1)S(1)}, s16[272,128]{1,0:T(8,128)(2,1)S(1)}, u32[]{:S(2)}, u32[]{:S(2)}) collective-permute-start(s16[272,128]{1,0:T(8,128)(2,1)S(1)} %get-tuple-element.51), channel_id=1, source_target_pairs={{0,6},{2,4},{4,2},{6,0},{1,7},{3,5},{5,3},{7,1},{8,14},{10,12},{12... | collective-permute-start | bytes 208904 | tf_op jit(solution)/shard_map/ppermute | solution.py:398
  76.7 0.3 collective-permute-start.20
  77.1 1.6 %collective-permute-done.16.refs_0_ = s16[272,128]{1,0:T(8,128)(2,1)S(1)} collective-permute-done((s16[272,128]{1,0:T(8,128)(2,1)S(1)}, s16[272,128]{1,0:T(8,128)(2,1)S(1)}, u32[]{:S(2)}, u32[]{:S(2)}) %collective-permute-start.16) | collective-permute-done | bytes 69664 | tf_op jit(solution)/shard_map/ppermute | solution.py:398
  78.7 1.3 %attend_0_1.1 = bf16[512,256]{1,0:T(8,128)(2,1)S(1)} custom-call(s32[4]{0:T(128)S(1)} %pad_add_fusion.place_ref, bf16[256,2048]{1,0:T(8,128)(2,1)S(1)} %get-tuple-element.34.q_ref, bf16[256,2048]{1,0:T(8,128)(2,1)S(1)} %collective-permute-done.3.q_sib_ref, bf16[256,2048]{1,0:T(8,128)(2,1)S(1)} %get-tuple-element.29.k_ref, ...), custom_call_target="tpu_custom_call" | custom-call | flops 201326592 | bytes 1048576 | tf_op jit(solution)/shard_map/attend_0_1/pallas_call | solution.py:321
  80.0 2.5 %collective-permute-start.17 = (bf16[512,256]{1,0:T(8,128)(2,1)S(1)}, bf16[512,256]{1,0:T(8,128)(2,1)S(1)}, u32[]{:S(2)}, u32[]{:S(2)}) collective-permute-start(bf16[512,256]{1,0:T(8,128)(2,1)S(1)} %attend_0_1.1), channel_id=1, source_target_pairs={{0,2},{2,0},{1,3},{3,1},{4,6},{6,4},{5,7},{7,5},{8,10},{10,8},{9,1... | collective-permute-start | bytes 786440 | tf_op jit(solution)/shard_map/ppermute | solution.py:398
  82.6 0.0 collective-permute-done.18.refs_0_
  82.6 1.3 %attend_0_3.1 = bf16[512,256]{1,0:T(8,128)(2,1)S(1)} custom-call(s32[4]{0:T(128)S(1)} %pad_add_fusion.place_ref, bf16[256,2048]{1,0:T(8,128)(2,1)S(1)} %get-tuple-element.34.q_ref, bf16[256,2048]{1,0:T(8,128)(2,1)S(1)} %collective-permute-done.3.q_sib_ref, bf16[256,2048]{1,0:T(8,128)(2,1)S(1)} %get-tuple-element.29.k_ref, ...), custom_call_target="tpu_custom_call" | custom-call | flops 201326592 | bytes 1048576 | tf_op jit(solution)/shard_map/attend_0_3/pallas_call | solution.py:321
  83.9 0.1 collective-permute-start.19
  84.0 1.5 %collective-permute-start.21 = (f32[2,128,128]{2,1,0:T(8,128)S(1)}, f32[2,128,128]{2,1,0:T(8,128)S(1)}, u32[]{:S(2)}, u32[]{:S(2)}) collective-permute-start(f32[2,128,128]{2,1,0:T(8,128)S(1)} %get-tuple-element.55), channel_id=1, source_target_pairs={{0,4},{4,0},{1,5},{5,1},{2,6},{6,2},{3,7},{7,3},{8,12},{12,8},{9,1... | collective-permute-start | bytes 393224 | tf_op jit(solution)/shard_map/ppermute | solution.py:398
  85.6 0.0 collective-permute-done.20.refs_1_
  85.6 0.5 collective-permute-start.14
  86.1 2.9 %collective-permute-done.21.refs_3_ = f32[2,128,128]{2,1,0:T(8,128)S(1)} collective-permute-done((f32[2,128,128]{2,1,0:T(8,128)S(1)}, f32[2,128,128]{2,1,0:T(8,128)S(1)}, u32[]{:S(2)}, u32[]{:S(2)}) %collective-permute-start.21) | collective-permute-done | bytes 131104 | tf_op jit(solution)/shard_map/ppermute | solution.py:398
  89.0 1.5 %collective-permute-start.15 = (s16[272,128]{1,0:T(8,128)(2,1)S(1)}, s16[272,128]{1,0:T(8,128)(2,1)S(1)}, u32[]{:S(2)}, u32[]{:S(2)}) collective-permute-start(s16[272,128]{1,0:T(8,128)(2,1)S(1)} %get-tuple-element.49), channel_id=1, source_target_pairs={{0,4},{2,6},{4,0},{6,2},{1,5},{3,7},{5,1},{7,3},{8,12},{10,14},{12... | collective-permute-start | bytes 208904 | tf_op jit(solution)/shard_map/ppermute | solution.py:398
  90.5 1.4 %assemble_cache.1 = f32[1,8,128,128]{3,2,1,0:T(8,128)} custom-call(s32[4]{0:T(128)S(1)} %pad_add_fusion.place_ref, f32[2,128,128]{2,1,0:T(8,128)S(1)} %get-tuple-element.52.refs_0_, f32[2,128,128]{2,1,0:T(8,128)S(1)} %collective-permute-done.20.refs_1_, f32[2,128,128]{2,1,0:T(8,128)S(1)} %get-tuple-element.54.refs_2_, ...), custom_call_target="tpu_custom_call" | custom-call | tf_op jit(solution)/shard_map/assemble_cache/pallas_call | solution.py:383
  91.9 0.0 collective-permute-done.14.refs_1_
  91.9 1.9 %attend_0_0_2.1.refs_0_ = bf16[512,512]{1,0:T(8,128)(2,1)S(1)} custom-call(s32[4]{0:T(128)S(1)} %pad_add_fusion.place_ref, bf16[256,2048]{1,0:T(8,128)(2,1)S(1)} %get-tuple-element.34.q_ref, bf16[256,2048]{1,0:T(8,128)(2,1)S(1)} %collective-permute-done.3.q_sib_ref, bf16[256,2048]{1,0:T(8,128)(2,1)S(1)} %get-tuple-element.29.k_ref, ...), custom_call_target="tpu_custom_call" | custom-call | flops 402653184 | bytes 2097152 | tf_op jit(solution)/shard_map/attend_0_0_2/pallas_call | solution.py:321
  93.8 0.0 collective-permute-done.15.refs_1_
  93.8 1.9 %attend_1_0_2.1.refs_1_ = bf16[512,512]{1,0:T(8,128)(2,1)S(1)} custom-call(s32[4]{0:T(128)S(1)} %pad_add_fusion.place_ref, bf16[256,2048]{1,0:T(8,128)(2,1)S(1)} %get-tuple-element.34.q_ref, bf16[256,2048]{1,0:T(8,128)(2,1)S(1)} %collective-permute-done.3.q_sib_ref, bf16[256,2048]{1,0:T(8,128)(2,1)S(1)} %get-tuple-element.29.k_ref, ...), custom_call_target="tpu_custom_call" | custom-call | flops 402653184 | bytes 2097152 | tf_op jit(solution)/shard_map/attend_1_0_2/pallas_call | solution.py:321
  95.7 0.0 collective-permute-done.17.refs_2_
  95.7 0.0 collective-permute-done.19.refs_3_
  95.7 1.7 %assemble.1.refs_1_ = bf16[1024,1024]{1,0:T(8,128)(2,1)} custom-call(s32[4]{0:T(128)S(1)} %pad_add_fusion.place_ref, bf16[512,512]{1,0:T(8,128)(2,1)S(1)} %attend_0_0_2.1.refs_0_, bf16[512,512]{1,0:T(8,128)(2,1)S(1)} %attend_1_0_2.1.refs_1_, bf16[512,256]{1,0:T(8,128)(2,1)S(1)} %collective-permute-done.17.refs_2_, ...), custom_call_target="tpu_custom_call" | custom-call | tf_op jit(solution)/shard_map/assemble/pallas_call | solution.py:360
  97.4 0.0 collective-permute-done.11.refs_0_
  97.4 1.4 %finish.1 = bf16[1024,1024]{1,0:T(8,128)(2,1)} custom-call(s32[4]{0:T(128)S(1)} %pad_add_fusion.place_ref, bf16[512,512]{1,0:T(8,128)(2,1)S(1)} %collective-permute-done.11.refs_0_, bf16[1024,1024]{1,0:T(8,128)(2,1)} %assemble.1.refs_1_), custom_call_target="tpu_custom_call", output_to_operand_aliasing={{}: (2, {})} | custom-call | tf_op jit(solution)/shard_map/finish/pallas_call | solution.py:360
  (4 shorter events, 0.0 us)
Async XLA Ops:
  0.7 8.6 %copy-start.2 = (f32[1024]{0:T(1024)S(1)}, f32[1024]{0:T(1024)}, u32[]{:S(2)}) copy-start(f32[1024]{0:T(1024)} %param.9) | copy-start | bytes 12292
  8.8 5.1 %collective-permute-start = (bf16[256,2048]{1,0:T(8,128)(2,1)}, bf16[256,2048]{1,0:T(8,128)(2,1)S(1)}, u32[]{:S(2)}, u32[]{:S(2)}) collective-permute-start(bf16[256,2048]{1,0:T(8,128)(2,1)} %get-tuple-element.30), channel_id=1, source_target_pairs={{0,1},{1,0},{2,3},{3,2},{4,5},{5,4},{6,7},{7,6},{8,9},{9,8},{10,11... | collective-permute-start | bytes 3145736 | tf_op jit(solution)/shard_map/ppermute | solution.py:398
  9.2 4.6 %collective-permute-start.1 = (bf16[256,2048]{1,0:T(8,128)(2,1)}, bf16[256,2048]{1,0:T(8,128)(2,1)S(1)}, u32[]{:S(2)}, u32[]{:S(2)}) collective-permute-start(bf16[256,2048]{1,0:T(8,128)(2,1)} %get-tuple-element.32), channel_id=1, source_target_pairs={{0,1},{1,0},{2,3},{3,2},{4,5},{5,4},{6,7},{7,6},{8,9},{9,8},{10,11... | collective-permute-start | bytes 3145736 | tf_op jit(solution)/shard_map/ppermute | solution.py:398
  9.3 4.6 %collective-permute-start.2 = (f32[1,1024]{1,0:T(1,128)S(1)}, f32[1,1024]{1,0:T(1,128)S(1)}, u32[]{:S(2)}, u32[]{:S(2)}) collective-permute-start(f32[1,1024]{1,0:T(1,128)S(1)} %bitcast.5), channel_id=1, source_target_pairs={{0,2},{2,0},{1,3},{3,1},{4,6},{6,4},{5,7},{7,5},{8,10},{10,8},{9,1... | collective-permute-start | bytes 12296 | tf_op jit(solution)/shard_map/ppermute | solution.py:398
  13.9 1.2 %copy-start = (bf16[256,2048]{1,0:T(8,128)(2,1)S(1)}, bf16[256,2048]{1,0:T(8,128)(2,1)}, u32[]{:S(2)}) copy-start(bf16[256,2048]{1,0:T(8,128)(2,1)} %get-tuple-element.31.v_ref) | copy-start | bytes 3145732
  24.4 31.3 %copy-start.1 = (bf16[256,2048]{1,0:T(8,128)(2,1)S(1)}, bf16[256,2048]{1,0:T(8,128)(2,1)}, u32[]{:S(2)}) copy-start(bf16[256,2048]{1,0:T(8,128)(2,1)} %get-tuple-element.31.v_ref) | copy-start | bytes 3145732
  24.4 31.3 %collective-permute-start.3 = (bf16[256,2048]{1,0:T(8,128)(2,1)}, bf16[256,2048]{1,0:T(8,128)(2,1)S(1)}, u32[]{:S(2)}, u32[]{:S(2)}) collective-permute-start(bf16[256,2048]{1,0:T(8,128)(2,1)} %get-tuple-element.35), channel_id=1, source_target_pairs={{0,1},{1,0},{2,3},{3,2},{4,5},{5,4},{6,7},{7,6},{8,9},{9,8},{10,11... | collective-permute-start | bytes 3145736 | tf_op jit(solution)/shard_map/ppermute | solution.py:398
  24.4 6.5 %collective-permute-start.4 = (s16[528,128]{1,0:T(8,128)(2,1)S(1)}, s16[528,128]{1,0:T(8,128)(2,1)S(1)}, u32[]{:S(2)}, u32[]{:S(2)}) collective-permute-start(s16[528,128]{1,0:T(8,128)(2,1)S(1)} %get-tuple-element.37), channel_id=1, source_target_pairs={{0,2},{2,0},{4,6},{6,4},{1,3},{3,1},{5,7},{7,5},{8,10},{10,8},{12,... | collective-permute-start | bytes 405512 | tf_op jit(solution)/shard_map/ppermute | solution.py:398
  26.8 6.4 %collective-permute-start.5 = (s16[528,128]{1,0:T(8,128)(2,1)S(1)}, s16[528,128]{1,0:T(8,128)(2,1)S(1)}, u32[]{:S(2)}, u32[]{:S(2)}) collective-permute-start(s16[528,128]{1,0:T(8,128)(2,1)S(1)} %get-tuple-element.38), channel_id=1, source_target_pairs={{0,4},{2,6},{4,0},{6,2},{1,5},{3,7},{5,1},{7,3},{8,12},{10,14},{12... | collective-permute-start | bytes 405512 | tf_op jit(solution)/shard_map/ppermute | solution.py:398
  28.3 6.7 %collective-permute-start.6 = (s16[528,128]{1,0:T(8,128)(2,1)S(1)}, s16[528,128]{1,0:T(8,128)(2,1)S(1)}, u32[]{:S(2)}, u32[]{:S(2)}) collective-permute-start(s16[528,128]{1,0:T(8,128)(2,1)S(1)} %get-tuple-element.39), channel_id=1, source_target_pairs={{0,6},{2,4},{4,2},{6,0},{1,7},{3,5},{5,3},{7,1},{8,14},{10,12},{12... | collective-permute-start | bytes 405512 | tf_op jit(solution)/shard_map/ppermute | solution.py:398
  35.1 5.6 %collective-permute-start.7 = (s16[272,128]{1,0:T(8,128)(2,1)S(1)}, s16[272,128]{1,0:T(8,128)(2,1)S(1)}, u32[]{:S(2)}, u32[]{:S(2)}) collective-permute-start(s16[272,128]{1,0:T(8,128)(2,1)S(1)} %get-tuple-element.40), channel_id=1, source_target_pairs={{0,8},{8,16},{16,24},{1,9},{9,17},{17,25},{2,10},{10,18},{18,26},{... | collective-permute-start | bytes 208904 | tf_op jit(solution)/shard_map/ppermute | solution.py:405
  40.8 7.2 %collective-permute-start.8 = (s16[272,128]{1,0:T(8,128)(2,1)S(1)}, s16[272,128]{1,0:T(8,128)(2,1)S(1)}, u32[]{:S(2)}, u32[]{:S(2)}) collective-permute-start(s16[272,128]{1,0:T(8,128)(2,1)S(1)} %levels_so_far_1_1.1), channel_id=1, source_target_pairs={{0,16},{8,24},{1,17},{9,25},{2,18},{10,26},{3,19},{11,27},{4,20},{... | collective-permute-start | bytes 208904 | tf_op jit(solution)/shard_map/ppermute | solution.py:405
  49.0 4.4 %collective-permute-start.9 = (s16[272,128]{1,0:T(8,128)(2,1)S(1)}, s16[272,128]{1,0:T(8,128)(2,1)S(1)}, u32[]{:S(2)}, u32[]{:S(2)}) collective-permute-start(s16[272,128]{1,0:T(8,128)(2,1)S(1)} %get-tuple-element.42), channel_id=1, source_target_pairs={{0,2},{2,0},{4,6},{6,4},{1,3},{3,1},{5,7},{7,5},{8,10},{10,8},{12,... | collective-permute-start | bytes 208904 | tf_op jit(solution)/shard_map/ppermute | solution.py:398
  50.6 5.2 %collective-permute-start.10 = (s16[272,128]{1,0:T(8,128)(2,1)S(1)}, s16[272,128]{1,0:T(8,128)(2,1)S(1)}, u32[]{:S(2)}, u32[]{:S(2)}) collective-permute-start(s16[272,128]{1,0:T(8,128)(2,1)S(1)} %get-tuple-element.43), channel_id=1, source_target_pairs={{0,6},{2,4},{4,2},{6,0},{1,7},{3,5},{5,3},{7,1},{8,14},{10,12},{12... | collective-permute-start | bytes 208904 | tf_op jit(solution)/shard_map/ppermute | solution.py:398
  57.6 39.8 %collective-permute-start.11 = (bf16[512,512]{1,0:T(8,128)(2,1)S(1)}, bf16[512,512]{1,0:T(8,128)(2,1)S(1)}, u32[]{:S(2)}, u32[]{:S(2)}) collective-permute-start(bf16[512,512]{1,0:T(8,128)(2,1)S(1)} %attend_1_1_3.1), channel_id=1, source_target_pairs={{0,2},{2,0},{1,3},{3,1},{4,6},{6,4},{5,7},{7,5},{8,10},{10,8},{9,1... | collective-permute-start | bytes 1572872 | tf_op jit(solution)/shard_map/ppermute | solution.py:398
  58.3 5.9 %collective-permute-start.12 = (s16[272,128]{1,0:T(8,128)(2,1)S(1)}, s16[272,128]{1,0:T(8,128)(2,1)S(1)}, u32[]{:S(2)}, u32[]{:S(2)}) collective-permute-start(s16[272,128]{1,0:T(8,128)(2,1)S(1)} %get-tuple-element.44), channel_id=1, source_target_pairs={{0,8},{8,16},{16,24},{1,9},{9,17},{17,25},{2,10},{10,18},{18,26},{... | collective-permute-start | bytes 208904 | tf_op jit(solution)/shard_map/ppermute | solution.py:405
  64.3 8.3 %collective-permute-start.13 = (s16[272,128]{1,0:T(8,128)(2,1)S(1)}, s16[272,128]{1,0:T(8,128)(2,1)S(1)}, u32[]{:S(2)}, u32[]{:S(2)}) collective-permute-start(s16[272,128]{1,0:T(8,128)(2,1)S(1)} %levels_so_far_0_1.1), channel_id=1, source_target_pairs={{0,16},{8,24},{1,17},{9,25},{2,18},{10,26},{3,19},{11,27},{4,20},{... | collective-permute-start | bytes 208904 | tf_op jit(solution)/shard_map/ppermute | solution.py:405
  73.5 5.2 %collective-permute-start.16 = (s16[272,128]{1,0:T(8,128)(2,1)S(1)}, s16[272,128]{1,0:T(8,128)(2,1)S(1)}, u32[]{:S(2)}, u32[]{:S(2)}) collective-permute-start(s16[272,128]{1,0:T(8,128)(2,1)S(1)} %get-tuple-element.50), channel_id=1, source_target_pairs={{0,2},{2,0},{4,6},{6,4},{1,3},{3,1},{5,7},{7,5},{8,10},{10,8},{12,... | collective-permute-start | bytes 208904 | tf_op jit(solution)/shard_map/ppermute | solution.py:398
  75.3 7.3 %collective-permute-start.18 = (s16[272,128]{1,0:T(8,128)(2,1)S(1)}, s16[272,128]{1,0:T(8,128)(2,1)S(1)}, u32[]{:S(2)}, u32[]{:S(2)}) collective-permute-start(s16[272,128]{1,0:T(8,128)(2,1)S(1)} %get-tuple-element.51), channel_id=1, source_target_pairs={{0,6},{2,4},{4,2},{6,0},{1,7},{3,5},{5,3},{7,1},{8,14},{10,12},{12... | collective-permute-start | bytes 208904 | tf_op jit(solution)/shard_map/ppermute | solution.py:398
  76.7 8.8 %collective-permute-start.20 = (f32[2,128,128]{2,1,0:T(8,128)S(1)}, f32[2,128,128]{2,1,0:T(8,128)S(1)}, u32[]{:S(2)}, u32[]{:S(2)}) collective-permute-start(f32[2,128,128]{2,1,0:T(8,128)S(1)} %get-tuple-element.53), channel_id=1, source_target_pairs={{0,4},{4,0},{1,5},{5,1},{2,6},{6,2},{3,7},{7,3},{8,12},{12,8},{9,1... | collective-permute-start | bytes 393224 | tf_op jit(solution)/shard_map/ppermute | solution.py:398
  80.0 15.6 %collective-permute-start.17 = (bf16[512,256]{1,0:T(8,128)(2,1)S(1)}, bf16[512,256]{1,0:T(8,128)(2,1)S(1)}, u32[]{:S(2)}, u32[]{:S(2)}) collective-permute-start(bf16[512,256]{1,0:T(8,128)(2,1)S(1)} %attend_0_1.1), channel_id=1, source_target_pairs={{0,2},{2,0},{1,3},{3,1},{4,6},{6,4},{5,7},{7,5},{8,10},{10,8},{9,1... | collective-permute-start | bytes 786440 | tf_op jit(solution)/shard_map/ppermute | solution.py:398
  83.9 11.8 %collective-permute-start.19 = (bf16[512,256]{1,0:T(8,128)(2,1)S(1)}, bf16[512,256]{1,0:T(8,128)(2,1)S(1)}, u32[]{:S(2)}, u32[]{:S(2)}) collective-permute-start(bf16[512,256]{1,0:T(8,128)(2,1)S(1)} %attend_0_3.1), channel_id=1, source_target_pairs={{0,2},{2,0},{1,3},{3,1},{4,6},{6,4},{5,7},{7,5},{8,10},{10,8},{9,1... | collective-permute-start | bytes 786440 | tf_op jit(solution)/shard_map/ppermute | solution.py:398
  84.0 5.0 %collective-permute-start.21 = (f32[2,128,128]{2,1,0:T(8,128)S(1)}, f32[2,128,128]{2,1,0:T(8,128)S(1)}, u32[]{:S(2)}, u32[]{:S(2)}) collective-permute-start(f32[2,128,128]{2,1,0:T(8,128)S(1)} %get-tuple-element.55), channel_id=1, source_target_pairs={{0,4},{4,0},{1,5},{5,1},{2,6},{6,2},{3,7},{7,3},{8,12},{12,8},{9,1... | collective-permute-start | bytes 393224 | tf_op jit(solution)/shard_map/ppermute | solution.py:398
  85.6 6.3 %collective-permute-start.14 = (s16[272,128]{1,0:T(8,128)(2,1)S(1)}, s16[272,128]{1,0:T(8,128)(2,1)S(1)}, u32[]{:S(2)}, u32[]{:S(2)}) collective-permute-start(s16[272,128]{1,0:T(8,128)(2,1)S(1)} %get-tuple-element.47), channel_id=1, source_target_pairs={{0,4},{2,6},{4,0},{6,2},{1,5},{3,7},{5,1},{7,3},{8,12},{10,14},{12... | collective-permute-start | bytes 208904 | tf_op jit(solution)/shard_map/ppermute | solution.py:398
  89.0 4.7 %collective-permute-start.15 = (s16[272,128]{1,0:T(8,128)(2,1)S(1)}, s16[272,128]{1,0:T(8,128)(2,1)S(1)}, u32[]{:S(2)}, u32[]{:S(2)}) collective-permute-start(s16[272,128]{1,0:T(8,128)(2,1)S(1)} %get-tuple-element.49), channel_id=1, source_target_pairs={{0,4},{2,6},{4,0},{6,2},{1,5},{3,7},{5,1},{7,3},{8,12},{10,14},{12... | collective-permute-start | bytes 208904 | tf_op jit(solution)/shard_map/ppermute | solution.py:398

commit v4 on v3

v4 whole, which is shorter than its diff:
```python
import functools

import jax
import jax.numpy as jnp
from jax import lax
from jax.experimental import pallas as pl
from jax.experimental.pallas import tpu as pltpu
from jax.sharding import Mesh
from jax.sharding import PartitionSpec as P

HD = 128
SCORE_SCALE = HD ** (-0.5)
CORES = 2
VMEM_BYTES = 24 * 1024 * 1024
DECODE_VMEM_BYTES = 52 * 1024 * 1024
PAD = 16
TOP = 32767.0

VMEM = pl.BlockSpec(memory_space=pltpu.VMEM)
SMEM = pl.BlockSpec(memory_space=pltpu.SMEM)
HBM = pl.BlockSpec(memory_space=pltpu.HBM)
ANY = pl.BlockSpec(memory_space=pl.ANY)


def params(vmem=VMEM_BYTES):
    return pltpu.CompilerParams(vmem_limit_bytes=vmem)


def cost(flops, bytes_accessed):
    return pl.CostEstimate(flops=flops, bytes_accessed=bytes_accessed, transcendentals=0)


class Plan:
    def __init__(self, mesh, rows, model):
        n_seq, n_head = mesh.shape["seq"], mesh.shape["head"]
        self.n_y = n_head // CORES
        self.width = model // n_head
        group = self.width // HD
        self.n_inner = 2 if n_seq % 2 == 0 and group % 2 == 0 else 1
        self.n_outer = n_seq // self.n_inner
        self.halves = 2 if group // self.n_inner % 2 == 0 else 1
        self.each = group // (self.n_inner * self.halves)
        self.plane = self.n_inner * self.n_y
        self.rows = rows
        self.block = rows * n_head
        self.piece = self.each * HD


def counts_of(spikes, names):
    one, two = jnp.ones_like(spikes), jnp.full_like(spikes, 2)
    zero = jnp.zeros_like(spikes)

    def ternary(rest, unit):
        return jnp.where(rest >= 2 * unit, two, jnp.where(rest >= unit, one, zero))

    counts = {"value": ternary(spikes, 9)}
    if names != ("value",):
        rest = spikes - 9 * counts["value"]
        counts["key"] = ternary(rest, 3)
        if "query" in names:
            counts["query"] = rest - 3 * counts["key"]
    return counts


def decode(plan, place, spikes, operands):
    names = tuple(operands)
    rows, model = spikes.shape
    step = min(rows, 32)
    chunks = rows // step
    width = plan.width
    n = len(names)

    def kernel(place_ref, *refs):
        sources, outs = refs[: 1 + n], refs[1 + n : 1 + 3 * n]
        buffers, sems = refs[1 + 3 * n : -1], refs[-1]

        def fetch(chunk, index):
            at = pl.ds(chunk * step, step)
            return pltpu.make_async_copy(
                sources[index].at[at], buffers[index].at[at], sems.at[chunk, index]
            )

        for chunk in range(chunks):
            for index in range(1 + n):
                fetch(chunk, index).start()

        @pl.loop(0, chunks)
        def _(chunk):
            for index in range(1 + n):
                fetch(chunk, index).wait()
            at = pl.ds(pl.multiple_of(chunk * step, step), step)
            for y in range(plan.n_y):
                for side in range(CORES):
                    of = place_ref[0] if side == 0 else 1 - place_ref[0]
                    columns = pl.ds(pl.multiple_of((y * CORES + of) * width, width), width)
                    codes = buffers[0][at, columns].astype(jnp.float32).astype(jnp.bfloat16)
                    counts = counts_of(codes, names)
                    for index, name in enumerate(names):
                        outs[2 * index + side][at, y * width : (y + 1) * width] = (
                            buffers[1 + index][at, columns] * counts[name]
                        )

    return pl.pallas_call(
        kernel,
        out_shape=[jax.ShapeDtypeStruct((rows, plan.n_y * width), jnp.bfloat16)] * (2 * n),
        in_specs=[SMEM] + [HBM] * (1 + n),
        out_specs=[VMEM] * (2 * n),
        scratch_shapes=[pltpu.VMEM((rows, model), jnp.int32)]
        + [pltpu.VMEM((rows, model), jnp.bfloat16)] * n
        + [pltpu.SemaphoreType.DMA((chunks, 1 + n))],
        compiler_params=params(DECODE_VMEM_BYTES),
        cost_estimate=cost(rows * model * 4, rows * model * (4 + 4 * n)),
        name="decode",
    )(place, spikes, *operands.values())


def contract_rows(left, right):
    return lax.dot_general(
        left, right, (((0,), (0,)), ((), ())), preferred_element_type=jnp.float32
    )


def contract_columns(left, right):
    return lax.dot_general(
        left, right, (((1,), (1,)), ((), ())), preferred_element_type=jnp.float32
    )


def code(states, ref):
    line = lax.broadcasted_iota(jnp.int32, (PAD, HD), 0)
    exponents = jnp.zeros((PAD, HD), jnp.float32)
    for i, state in enumerate(states):
        top = jnp.max(jnp.abs(state), axis=0, keepdims=True)
        exponent = jnp.floor(jnp.log2(jnp.maximum(top, 1e-30))) + 1
        scaled = jnp.round(state * jnp.exp2(15 - exponent))
        scaled = jnp.clip(scaled, -TOP, TOP)
        ref[i * HD : (i + 1) * HD] = scaled.astype(jnp.int32).astype(jnp.int16)
        exponents = jnp.where(line == i, exponent, exponents)
    ref[len(states) * HD :] = exponents.astype(jnp.int32).astype(jnp.int16)


def decoded(ref):
    count = ref.shape[0] // HD
    exponents = ref[count * HD :].astype(jnp.int32).astype(jnp.float32)
    return [
        ref[i * HD : (i + 1) * HD].astype(jnp.int32).astype(jnp.float32)
        * jnp.exp2(exponents[i : i + 1] - 15)
        for i in range(count)
    ]


def plus(left, right):
    return [a + b for a, b in zip(left, right)]


def coded_shape(heads):
    return jax.ShapeDtypeStruct((heads * HD + PAD, HD), jnp.int16)


def states_shape(*lead):
    return jax.ShapeDtypeStruct((*lead, HD, HD), jnp.float32)


def owned_columns(plan, place_ref, offset, half, i):
    x = place_ref[1] ^ (offset // plan.n_y)
    y = place_ref[2] ^ (offset % plan.n_y)
    start = (((y * plan.halves + half) * plan.n_inner + x) * plan.each + i) * HD
    return pl.ds(pl.multiple_of(start, HD), HD)


def chunk_states(plan, place, key, value, half, after):
    def kernel(place_ref, k_ref, k_sib_ref, v_ref, v_sib_ref, *refs):
        own_ref, first_ref, *send_refs = refs[len(after) :]
        is_first = jnp.full((HD, HD), place_ref[0], jnp.int32) == 0
        for offset in (*range(1, plan.plane), 0):
            states = []
            for i in range(plan.each):
                at = owned_columns(plan, place_ref, offset, half, i)
                mine = contract_rows(v_ref[:, at], k_ref[:, at])
                sib = contract_rows(v_sib_ref[:, at], k_sib_ref[:, at])
                first_ref[offset, i] = jnp.where(is_first, mine, sib)
                states.append(mine + sib)
            if offset:
                code(states, send_refs[offset - 1])
            else:
                for i, state in enumerate(states):
                    own_ref[i] = state

    heads = plan.plane * plan.each
    return pl.pallas_call(
        kernel,
        out_shape=[states_shape(plan.each), states_shape(plan.plane, plan.each)]
        + [coded_shape(plan.each)] * (plan.plane - 1),
        in_specs=[SMEM] + [VMEM] * 4 + [ANY] * len(after),
        out_specs=[VMEM] * (1 + plan.plane),
        compiler_params=params(),
        cost_estimate=cost(
            4 * plan.rows * HD * HD * heads, 8 * plan.rows * HD * heads + 6 * heads * HD * HD
        ),
        name=f"chunk_states_{half}",
    )(place, *key, *value, *after)


def level_states(plan, own, others, half, after):
    def kernel(own_ref, *refs):
        total = [own_ref[i] for i in range(plan.each)]
        for ref in refs[: len(others)]:
            total = plus(total, decoded(ref))
        code(total, refs[-1])

    return pl.pallas_call(
        kernel,
        out_shape=coded_shape(plan.each),
        in_specs=[VMEM] * plan.plane + [ANY] * len(after),
        out_specs=VMEM,
        compiler_params=params(),
        cost_estimate=cost(0, plan.plane * plan.each * HD * HD * 2),
        name=f"level_states_{half}",
    )(own, *others, *after)


def carried(plan, place_ref, own, others, levels, offsets):
    x, y = place_ref[1], place_ref[2]
    here = x * plan.n_y + y
    earlier = [jnp.zeros((HD, HD), jnp.float32)] * plan.each
    for ref in levels:
        earlier = plus(earlier, decoded(ref))
    states = [[own[i] for i in range(plan.each)]] + [decoded(ref) for ref in others]

    def add(totals, keep_of):
        for offset, terms in enumerate(states):
            keep = jnp.full((HD, HD), keep_of(here ^ offset), jnp.int32) == 1
            totals = plus(totals, [jnp.where(keep, s, 0.0) for s in terms])
        return totals

    before = [add(earlier, lambda chip: (chip < here ^ o).astype(jnp.int32)) for o in offsets]
    blocks = [
        add(earlier, lambda chip: (chip // plan.n_y <= x ^ o).astype(jnp.int32))
        for o in range(plan.n_inner)
    ]
    return before, blocks


def carries(plan, place, own, others, levels, half, offsets, after):
    n_others, n_levels = len(others), len(levels)

    def kernel(place_ref, own_ref, *refs):
        before, _ = carried(
            plan, place_ref, own_ref, refs[:n_others], refs[n_others : n_others + n_levels], offsets
        )
        for states, ref in zip(before, refs[n_others + n_levels + len(after) :]):
            code(states, ref)

    return pl.pallas_call(
        kernel,
        out_shape=[coded_shape(plan.each)] * len(offsets),
        in_specs=[SMEM] + [VMEM] * (1 + n_others + n_levels) + [ANY] * len(after),
        out_specs=[VMEM] * len(offsets),
        compiler_params=params(),
        cost_estimate=cost(0, (plan.plane * 4 + n_levels) * plan.each * HD * HD * 2),
        name=f"carries_{half}",
    )(place, own, *others, *levels, *after)


def own_carries(plan, place, own, others, levels, offsets, after):
    n_others, n_levels = len(others[0]), len(levels[0])
    each_half = 1 + n_others + n_levels

    def kernel(place_ref, *refs):
        outs = refs[plan.halves * each_half + len(after) :]
        befores = [[] for _ in offsets]
        for half in range(plan.halves):
            own_ref, *of_half = refs[half * each_half : (half + 1) * each_half]
            before, blocks = carried(
                plan, place_ref, own_ref, of_half[:n_others], of_half[n_others:], offsets
            )
            for all_states, states in zip(befores, before):
                all_states.extend(states)
            for offset, (totals, ref) in enumerate(zip(blocks, outs[len(offsets) :])):
                block = place_ref[3] * plan.n_inner + (place_ref[1] ^ offset)
                seen = jnp.full((1, HD), (block + 1) * plan.block, jnp.int32).astype(jnp.float32)
                for i, total in enumerate(totals):
                    ref[half, i] = total.T * lax.rsqrt(seen)
        for states, ref in zip(befores, outs):
            code(states, ref)

    operands = [a for h in range(plan.halves) for a in (own[h], *others[h], *levels[h])]
    return pl.pallas_call(
        kernel,
        out_shape=[coded_shape(plan.halves * plan.each)] * len(offsets)
        + [states_shape(plan.halves, plan.each)] * plan.n_inner,
        in_specs=[SMEM] + [VMEM] * len(operands) + [ANY] * len(after),
        out_specs=[VMEM] * (len(offsets) + plan.n_inner),
        compiler_params=params(),
        cost_estimate=cost(0, (plan.plane * 4 + n_levels) * plan.each * HD * HD * 4),
        name="own_carries",
    )(place, *operands, *after)


def attend(plan, place, query, key, value, carry, first, gain, half, offsets, after=()):
    rows = plan.rows

    def kernel(
        place_ref, q_ref, q_sib_ref, k_ref, k_sib_ref, v_ref, v_sib_ref, first_ref, gain_ref, *refs
    ):
        core = place_ref[0]
        out_ref = refs[-1]
        causal = lax.broadcasted_iota(jnp.int32, (rows, rows), 0) >= lax.broadcasted_iota(
            jnp.int32, (rows, rows), 1
        )
        is_second = jnp.full((HD, HD), core, jnp.int32) == 1

        def attended(q_ref, k_ref, v_ref, at, carried, gain):
            queries = q_ref[:, at]
            scores = contract_columns(queries, k_ref[:, at]) * SCORE_SCALE
            weights = jnp.where(causal, scores, 0.0).astype(jnp.bfloat16)
            raw = jnp.dot(weights, v_ref[:, at], preferred_element_type=jnp.float32)
            carried = carried * SCORE_SCALE
            high = carried.astype(jnp.bfloat16)
            low = (carried - high.astype(jnp.float32)).astype(jnp.bfloat16)
            both = contract_columns(queries, jnp.concatenate([high, low], axis=0))
            raw = raw + (both[:, :HD] + both[:, HD:])
            mean = jnp.mean(raw * raw, axis=-1, keepdims=True)
            return (raw * lax.rsqrt(mean + 1e-06) * gain).astype(jnp.bfloat16)

        for piece, offset in enumerate(offsets):
            x = place_ref[1] ^ (offset // plan.n_y)
            carry_states = decoded(refs[piece])
            skip = half * plan.each if len(carry_states) > plan.each else 0
            for i in range(plan.each):
                at = owned_columns(plan, place_ref, offset, half, i)
                start = ((half * plan.n_inner + x) * plan.each + i) * HD
                gain = gain_ref[:, pl.ds(pl.multiple_of(start, HD), HD)]
                out_at = slice(piece * plan.piece + i * HD, piece * plan.piece + (i + 1) * HD)
                first = first_ref[offset, i]
                mine = carry_states[skip + i] + jnp.where(is_second, first, 0.0)
                sib = carry_states[skip + i] + jnp.where(is_second, 0.0, first)
                out_ref[pl.ds(pl.multiple_of(core * rows, rows), rows), out_at] = attended(
                    q_ref, k_ref, v_ref, at, mine, gain
                )
                out_ref[pl.ds(pl.multiple_of((1 - core) * rows, rows), rows), out_at] = attended(
                    q_sib_ref, k_sib_ref, v_sib_ref, at, sib, gain
                )

    heads = len(offsets) * plan.each
    return pl.pallas_call(
        kernel,
        out_shape=jax.ShapeDtypeStruct((CORES * rows, heads * HD), jnp.bfloat16),
        in_specs=[SMEM] + [VMEM] * (8 + len(offsets)) + [ANY] * len(after),
        out_specs=VMEM,
        compiler_params=params(),
        cost_estimate=cost(
            heads * (8 * rows * rows * HD + 8 * rows * HD * HD), 16 * rows * heads * HD
        ),
        name=f"attend_{half}_" + "_".join(map(str, offsets)),
    )(place, *query, *key, *value, first, gain, *carry, *after)


def assemble(plan, place, parts, into=None):
    rows = CORES * plan.rows
    copies = [(n, piece, half, o) for n, (_, half, os) in enumerate(parts) for piece, o in enumerate(os)]

    def kernel(place_ref, *refs):
        out_ref, sems = refs[-2:]
        started = []
        for at, (n, piece, half, offset) in enumerate(copies):
            x = place_ref[1] ^ (offset // plan.n_y)
            y = place_ref[2] ^ (offset % plan.n_y)
            column = (half * plan.n_inner + x) * plan.piece
            to_rows = pl.ds(pl.multiple_of(y * rows, rows), rows)
            to_columns = pl.ds(pl.multiple_of(column, plan.piece), plan.piece)
            started.append(
                pltpu.make_async_copy(
                    refs[n].at[:, pl.ds(piece * plan.piece, plan.piece)],
                    out_ref.at[to_rows, to_columns],
                    sems.at[at],
                )
            )
            started[-1].start()
        for copy in started:
            copy.wait()

    arrays = [array for array, _, _ in parts]
    aliased = [] if into is None else [into]
    return pl.pallas_call(
        kernel,
        out_shape=jax.ShapeDtypeStruct((plan.n_y * rows, plan.width), jnp.bfloat16),
        in_specs=[SMEM] + [VMEM] * len(arrays) + [HBM] * len(aliased),
        out_specs=HBM,
        scratch_shapes=[pltpu.SemaphoreType.DMA((len(copies),))],
        input_output_aliases={1 + len(arrays): 0} if aliased else {},
        compiler_params=params(),
        name="assemble" if into is None else "finish",
    )(place, *arrays, *aliased)


def assemble_cache(plan, place, parts):
    group = plan.n_inner * plan.each

    def kernel(place_ref, *refs):
        for half in range(plan.halves):
            for offset, ref in enumerate(refs[:-1]):
                start = half * group + (place_ref[1] ^ offset) * plan.each
                refs[-1][0, pl.ds(start, plan.each)] = ref[half]

    return pl.pallas_call(
        kernel,
        out_shape=states_shape(1, plan.halves * group),
        in_specs=[SMEM] + [VMEM] * len(parts),
        out_specs=VMEM,
        compiler_params=params(),
        name="assemble_cache",
    )(place, *parts)


def per_device(plan, queries, keys, values, spikes, gain):
    place = jnp.stack([lax.axis_index(a) for a in ("core", "inner", "y", "outer")]).astype(jnp.int32)
    halves = range(plan.halves)

    def swap(array, axes, offset, size):
        return lax.ppermute(array, axes, [(i, i ^ offset) for i in range(size)])

    def in_level(array, offset):
        return swap(array, ("inner", "y"), offset, plan.plane)

    def to_later(array, distance):
        pairs = [(i, i + distance) for i in range(plan.n_outer - distance)]
        return lax.ppermute(array, "outer", pairs)

    gain = gain.reshape(1, plan.width)
    gains = [gain] + [swap(gain, "y", o, plan.n_y) for o in range(1, plan.n_y)]
    arrays = decode(plan, place, spikes, {"key": keys, "value": values, "query": queries})
    key, value, query = (
        (mine, swap(sibling, "core", 1, CORES)) for mine, sibling in zip(arrays[::2], arrays[1::2])
    )

    after = [*gains[1:], query[1]]
    own, first, others = [], [], []
    for half in halves:
        mine, parts, *sends = chunk_states(plan, place, key, value, half, after)
        own.append(mine)
        first.append(parts)
        others.append([in_level(a, o) for o, a in enumerate(sends, 1)])
        after = [mine]
    levels = []
    for half in halves:
        level = level_states(plan, own[half], others[half], half, after)
        levels.append([to_later(level, d) for d in range(plan.n_outer - 1, 0, -1)])
        after = [level]

    of_group = [list(range(y, plan.plane, plan.n_y)) for y in range(plan.n_y)]
    abroad = [o for offsets in of_group[1:] for o in offsets]

    def part_of(half, offsets, carry, after):
        return attend(
            plan,
            place,
            query,
            key,
            value,
            [carry[o] for o in offsets],
            first[half],
            gains[offsets[0] % plan.n_y],
            half,
            offsets,
            after,
        )

    carry = []
    for half in halves:
        sends = carries(plan, place, own[half], others[half], levels[half], half, abroad, after)
        carry.append({o: in_level(a, o) for o, a in zip(abroad, sends)})
        after = [sends[0]]
    parts = []
    for half in halves:
        for y in range(1, plan.n_y):
            part = part_of(half, of_group[y], carry[half], after)
            parts.append((swap(part, "y", y, plan.n_y), half, of_group[y]))
            after = [part]
    sends = own_carries(plan, place, own, others, levels, of_group[0], after)
    own_carry = {o: in_level(a, o) if o else a for o, a in zip(of_group[0], sends)}
    caches = [
        swap(a, "inner", o, plan.n_inner) if o else a
        for o, a in enumerate(sends[len(of_group[0]) :])
    ]
    early = []
    for half in halves:
        part = part_of(half, of_group[0], own_carry, after)
        early.append((part, half, of_group[0]))
        after = [part]
    out = assemble(plan, place, early + parts[:-1])
    out = assemble(plan, place, parts[-1:], out)
    return out, assemble_cache(plan, place, caches)


def solution(mesh):
    tokens = P(("outer", "inner", "y", "core"), None)
    seq, head = ("outer", "inner"), ("y", "core")

    def whole(queries, keys, values, spikes, gain):
        plan = Plan(mesh, spikes.shape[0] // mesh.size, spikes.shape[1])
        sizes = (plan.n_outer, plan.n_inner, plan.n_y, CORES)
        split = Mesh(mesh.devices.reshape(sizes), ("outer", "inner", "y", "core"))
        return jax.shard_map(
            functools.partial(per_device, plan),
            mesh=split,
            in_specs=(tokens, tokens, tokens, tokens, P(head)),
            out_specs=(P(seq, head), P(seq, head, None, None)),
            check_vma=False,
        )(queries, keys, values, spikes, gain)

    return whole
```

time: 99.5 us -> 74.1 us (0.74)
  waiting for transfers between devices: 24.3 us -> 11.8 us
  Pallas kernels: 32.3 us -> 24.8 us
  starting transfers between devices: 40.1 us -> 35.2 us
    pallas_call x2 -> x1, Pallas kernels: 15.3 us -> 7.26 us  [decode(): pl.pallas_call(kernel, out_shape=[jax.ShapeDtypeStruct((rows, plan.n_y *...]
    ppermute x4 -> x6, waiting for transfers between devices: 7.69 us -> 0.02 us  [to_later(): return lax.ppermute(array, 'outer', pairs)]
    ppermute x4 -> x6, starting transfers between devices: 19.3 us -> 13.6 us  [to_later(): return lax.ppermute(array, 'outer', pairs)]
    ppermute x18, waiting for transfers between devices: 16.6 us -> 11.8 us  [swap(): return lax.ppermute(array, axes, [(i, i ^ offset) for i in range(size)])]
    pallas_call x8, Pallas kernels: 5.63 us -> 6.93 us  [the longest x2 2.73 us: chunk_states(): pl.pallas_call(kernel, out_shape=[states_shape(plan.each), states_shape(p...]
    pallas_call x5 -> x4, Pallas kernels: 8.29 us -> 7.49 us  [attend(): pl.pallas_call(kernel, out_shape=jax.ShapeDtypeStruct((CORES * rows, head...]
  transfers between devices with their start and end apart: 22 -> 24, of which waited for: 12 -> 6; matrix products, arithmetic and copies ran while one was open for 0% -> 0% of each run, Pallas kernels for 12% -> 20%
where the time goes in v4:
time: 74.1 us; the launch traced here: 73.9 us
  starting transfers between devices  35.2 us (48%)
  Pallas kernels  24.8 us (33%)
  waiting for transfers between devices  11.8 us (16%)
  local copies, waits for them, and re-layouts  1.24 us (2%)
  between operations  0.86 us (1%)
    ppermute x18, starting transfers between devices, swap(): return lax.ppermute(array, axes, [(i, i ^ offset) for i in range(size)])  21.5 us
    ppermute x6, starting transfers between devices, to_later(): return lax.ppermute(array, 'outer', pairs)  13.6 us
    ppermute x18, waiting for transfers between devices, swap(): return lax.ppermute(array, axes, [(i, i ^ offset) for i in range(size)])  11.8 us
    pallas_call x4, Pallas kernels, attend(): pl.pallas_call(kernel, out_shape=jax.ShapeDtypeStruct((CORES * rows, head...  7.49 us
    pallas_call x1, Pallas kernels, decode(): pl.pallas_call(kernel, out_shape=[jax.ShapeDtypeStruct((rows, plan.n_y *...  7.26 us
    pallas_call x2, Pallas kernels, assemble(): pl.pallas_call(kernel, out_shape=jax.ShapeDtypeStruct((plan.n_y * rows, p...  3.08 us
    pallas_call x2, Pallas kernels, chunk_states(): pl.pallas_call(kernel, out_shape=[states_shape(plan.each), states_shape(p...  2.73 us
    pallas_call x2, Pallas kernels, carries(): pl.pallas_call(kernel, out_shape=[coded_shape(plan.each)] * len(offsets),...  1.5 us
  transfers between devices with their start and end apart: 24, of which 6 were waited for; matrix products, arithmetic and copies ran while one was open for 0% of the time, Pallas kernels for 20%

profile of v4, /device:TPU:0, one launch (start us, length us, event | category | flops | bytes accessed | tf_op | source)
XLA Modules:
  0.0 73.9 jit_solution(12995970700801189945)
XLA Ops:
  0.6 0.1 pad_add_fusion.place_ref
  0.7 7.3 %decode.1 = (bf16[256,2048]{1,0:T(8,128)(2,1)S(1)}, bf16[256,2048]{1,0:T(8,128)(2,1)}, bf16[256,2048]{1,0:T(8,128)(2,1)}, bf16[256,2048]{1,0:T(8,128)(2,1)}, bf1...) custom-call(s32[4]{0:T(128)S(1)} %pad_add_fusion.place_ref, s32[256,4096]{1,0:T(8,128)} %refs_0_.1, ...), custom_call_target="tpu_custom_call" | custom-call | flops 4194304 | bytes 16777216 | tf_op jit(solution)/shard_map/decode/pallas_call | solution.py:103
  8.0 0.5 collective-permute-start
  8.5 0.1 collective-permute-start.1
  8.6 0.4 collective-permute-start.2
  9.0 2.6 %collective-permute-start.3 = (f32[1,1024]{1,0:T(1,128)S(1)}, f32[1,1024]{1,0:T(1,128)S(1)}, u32[]{:S(2)}, u32[]{:S(2)}) collective-permute-start(f32[1,1024]{1,0:T(1,128)S(1)} %bitcast.5), channel_id=1, source_target_pairs={{0,2},{2,0},{1,3},{3,1},{4,6},{6,4},{5,7},{7,5},{8,10},{10,8},{9,1... | collective-permute-start | bytes 12296 | tf_op jit(solution)/shard_map/ppermute | solution.py:421
  11.6 1.6 %collective-permute-done.3.refs_0_.gain_ref = f32[1,1024]{1,0:T(1,128)S(1)} collective-permute-done((f32[1,1024]{1,0:T(1,128)S(1)}, f32[1,1024]{1,0:T(1,128)S(1)}, u32[]{:S(2)}, u32[]{:S(2)}) %collective-permute-start.3) | collective-permute-done | bytes 4128 | tf_op jit(solution)/shard_map/ppermute | solution.py:421
  13.2 0.0 collective-permute-done.refs_1_.q_sib_ref
  13.2 0.0 collective-permute-done.1.k_sib_ref
  13.2 0.8 %collective-permute-done.2.v_sib_ref = bf16[256,2048]{1,0:T(8,128)(2,1)S(1)} collective-permute-done((bf16[256,2048]{1,0:T(8,128)(2,1)}, bf16[256,2048]{1,0:T(8,128)(2,1)S(1)}, u32[]{:S(2)}, u32[]{:S(2)}) %collective-permute-start.2) | collective-permute-done | bytes 1048608 | tf_op jit(solution)/shard_map/ppermute | solution.py:421
  14.0 1.2 %copy-done = bf16[256,2048]{1,0:T(8,128)(2,1)S(1)} copy-done((bf16[256,2048]{1,0:T(8,128)(2,1)S(1)}, bf16[256,2048]{1,0:T(8,128)(2,1)}, u32[]{:S(2)}) %copy-start) | copy-done | bytes 1048600
  15.2 1.4 %chunk_states_0.1 = (f32[2,128,128]{2,1,0:T(8,128)S(1)}, f32[4,2,128,128]{3,2,1,0:T(8,128)S(1)}, s16[272,128]{1,0:T(8,128)(2,1)S(1)}, s16[272,128]{1,0:T(8,128)(2,1)S(1)}, s16[272,128]{1,0:T(8,128)(2,1)S(1)}) custom-call(s32[4]{0:T(128)S(1)} %pad_add_fusion.place_ref, bf16[256,2048]{1,0:T(8,128)(2,1)S(1)} %get-tuple-element.28.k_ref, ...), custom_call_target="tpu_custom_call" | custom-call | flops 134217728 | bytes 2883584 | tf_op jit(solution)/shard_map/chunk_states_0/pallas_call | solution.py:190
  16.6 3.0 %collective-permute-start.7 = (s16[272,128]{1,0:T(8,128)(2,1)S(1)}, s16[272,128]{1,0:T(8,128)(2,1)S(1)}, u32[]{:S(2)}, u32[]{:S(2)}) collective-permute-start(s16[272,128]{1,0:T(8,128)(2,1)S(1)} %get-tuple-element.38), channel_id=1, source_target_pairs={{0,2},{2,0},{4,6},{6,4},{1,3},{3,1},{5,7},{7,5},{8,10},{10,8},{12,... | collective-permute-start | bytes 208904 | tf_op jit(solution)/shard_map/ppermute | solution.py:421
  19.5 1.5 %collective-permute-start.8 = (s16[272,128]{1,0:T(8,128)(2,1)S(1)}, s16[272,128]{1,0:T(8,128)(2,1)S(1)}, u32[]{:S(2)}, u32[]{:S(2)}) collective-permute-start(s16[272,128]{1,0:T(8,128)(2,1)S(1)} %get-tuple-element.39), channel_id=1, source_target_pairs={{0,4},{2,6},{4,0},{6,2},{1,5},{3,7},{5,1},{7,3},{8,12},{10,14},{12... | collective-permute-start | bytes 208904 | tf_op jit(solution)/shard_map/ppermute | solution.py:421
  21.0 0.0 collective-permute-start.9
  21.1 1.4 %chunk_states_1.1 = (f32[2,128,128]{2,1,0:T(8,128)S(1)}, f32[4,2,128,128]{3,2,1,0:T(8,128)S(1)}, s16[272,128]{1,0:T(8,128)(2,1)S(1)}, s16[272,128]{1,0:T(8,128)(2,1)S(1)}, s16[272,128]{1,0:T(8,128)(2,1)S(1)}) custom-call(s32[4]{0:T(128)S(1)} %pad_add_fusion.place_ref, bf16[256,2048]{1,0:T(8,128)(2,1)S(1)} %get-tuple-element.28.k_ref, ...), custom_call_target="tpu_custom_call" | custom-call | flops 134217728 | bytes 2883584 | tf_op jit(solution)/shard_map/chunk_states_1/pallas_call | solution.py:190
  22.5 2.0 %collective-permute-start.4 = (s16[272,128]{1,0:T(8,128)(2,1)S(1)}, s16[272,128]{1,0:T(8,128)(2,1)S(1)}, u32[]{:S(2)}, u32[]{:S(2)}) collective-permute-start(s16[272,128]{1,0:T(8,128)(2,1)S(1)} %get-tuple-element.35), channel_id=1, source_target_pairs={{0,2},{2,0},{4,6},{6,4},{1,3},{3,1},{5,7},{7,5},{8,10},{10,8},{12,... | collective-permute-start | bytes 208904 | tf_op jit(solution)/shard_map/ppermute | solution.py:421
  24.5 1.5 %collective-permute-start.5 = (s16[272,128]{1,0:T(8,128)(2,1)S(1)}, s16[272,128]{1,0:T(8,128)(2,1)S(1)}, u32[]{:S(2)}, u32[]{:S(2)}) collective-permute-start(s16[272,128]{1,0:T(8,128)(2,1)S(1)} %get-tuple-element.36), channel_id=1, source_target_pairs={{0,4},{2,6},{4,0},{6,2},{1,5},{3,7},{5,1},{7,3},{8,12},{10,14},{12... | collective-permute-start | bytes 208904 | tf_op jit(solution)/shard_map/ppermute | solution.py:421
  26.0 0.0 collective-permute-done.7.refs_0_.refs_1_
  26.0 0.1 collective-permute-start.6
  26.0 0.0 collective-permute-done.8.refs_1_.refs_2_
  26.0 0.6 collective-permute-done.9.refs_2_.refs_3_
  26.7 0.1 level_states_0.1.refs_3_
  26.8 3.3 %collective-permute-start.15 = (s16[272,128]{1,0:T(8,128)(2,1)S(1)}, s16[272,128]{1,0:T(8,128)(2,1)S(1)}, u32[]{:S(2)}, u32[]{:S(2)}) collective-permute-start(s16[272,128]{1,0:T(8,128)(2,1)S(1)} %level_states_0.1.refs_3_), channel_id=1, source_target_pairs={{0,8},{8,16},{16,24},{1,9},{9,17},{17,25},{2,10},{10,18},{18,26},{... | collective-permute-start | bytes 208904 | tf_op jit(solution)/shard_map/ppermute | solution.py:428
  30.1 4.5 %collective-permute-start.14 = (s16[272,128]{1,0:T(8,128)(2,1)S(1)}, s16[272,128]{1,0:T(8,128)(2,1)S(1)}, u32[]{:S(2)}, u32[]{:S(2)}) collective-permute-start(s16[272,128]{1,0:T(8,128)(2,1)S(1)} %level_states_0.1.refs_3_), channel_id=1, source_target_pairs={{0,16},{8,24},{1,17},{9,25},{2,18},{10,26},{3,19},{11,27},{4,20},{... | collective-permute-start | bytes 208904 | tf_op jit(solution)/shard_map/ppermute | solution.py:428
  34.6 0.0 collective-permute-done.4.refs_0_.refs_8_
  34.6 1.3 %collective-permute-start.13 = (s16[272,128]{1,0:T(8,128)(2,1)S(1)}, s16[272,128]{1,0:T(8,128)(2,1)S(1)}, u32[]{:S(2)}, u32[]{:S(2)}) collective-permute-start(s16[272,128]{1,0:T(8,128)(2,1)S(1)} %level_states_0.1.refs_3_), channel_id=1, source_target_pairs={{0,24},{1,25},{2,26},{3,27},{4,28},{5,29},{6,30},{7,31}} | collective-permute-start | bytes 208904 | tf_op jit(solution)/shard_map/ppermute | solution.py:428
  35.9 0.0 collective-permute-done.5.refs_1_.refs_9_
  35.9 0.0 collective-permute-done.6.refs_2_.refs_10_
  36.0 0.1 level_states_1.1.refs_6_
  36.1 1.3 %collective-permute-start.12 = (s16[272,128]{1,0:T(8,128)(2,1)S(1)}, s16[272,128]{1,0:T(8,128)(2,1)S(1)}, u32[]{:S(2)}, u32[]{:S(2)}) collective-permute-start(s16[272,128]{1,0:T(8,128)(2,1)S(1)} %level_states_1.1.refs_6_), channel_id=1, source_target_pairs={{0,8},{8,16},{16,24},{1,9},{9,17},{17,25},{2,10},{10,18},{18,26},{... | collective-permute-start | bytes 208904 | tf_op jit(solution)/shard_map/ppermute | solution.py:428
  37.4 1.9 %collective-permute-start.11 = (s16[272,128]{1,0:T(8,128)(2,1)S(1)}, s16[272,128]{1,0:T(8,128)(2,1)S(1)}, u32[]{:S(2)}, u32[]{:S(2)}) collective-permute-start(s16[272,128]{1,0:T(8,128)(2,1)S(1)} %level_states_1.1.refs_6_), channel_id=1, source_target_pairs={{0,16},{8,24},{1,17},{9,25},{2,18},{10,26},{3,19},{11,27},{4,20},{... | collective-permute-start | bytes 208904 | tf_op jit(solution)/shard_map/ppermute | solution.py:428
  39.3 0.0 collective-permute-done.15.refs_5_.refs_6_
  39.3 1.3 %collective-permute-start.10 = (s16[272,128]{1,0:T(8,128)(2,1)S(1)}, s16[272,128]{1,0:T(8,128)(2,1)S(1)}, u32[]{:S(2)}, u32[]{:S(2)}) collective-permute-start(s16[272,128]{1,0:T(8,128)(2,1)S(1)} %level_states_1.1.refs_6_), channel_id=1, source_target_pairs={{0,24},{1,25},{2,26},{3,27},{4,28},{5,29},{6,30},{7,31}} | collective-permute-start | bytes 208904 | tf_op jit(solution)/shard_map/ppermute | solution.py:428
  40.6 0.0 collective-permute-done.14.refs_4_.refs_5_
  40.6 0.0 collective-permute-done.13.refs_3_.refs_4_
  40.6 0.8 %carries_0.1 = (s16[272,128]{1,0:T(8,128)(2,1)S(1)}, s16[272,128]{1,0:T(8,128)(2,1)S(1)}) custom-call(s32[4]{0:T(128)S(1)} %pad_add_fusion.place_ref, f32[2,128,128]{2,1,0:T(8,128)S(1)} %get-tuple-element.32.refs_0_.own_ref, s16[272,128]{1,0:T(8,128)(2,1)S(1)} %collective-permute-done.7.refs_0_.refs_1_, ...), custom_call_target="tpu_custom_call" | custom-call | bytes 1245184 | tf_op jit(solution)/shard_map/carries_0/pallas_call | solution.py:254
  41.4 1.8 %collective-permute-start.19 = (s16[272,128]{1,0:T(8,128)(2,1)S(1)}, s16[272,128]{1,0:T(8,128)(2,1)S(1)}, u32[]{:S(2)}, u32[]{:S(2)}) collective-permute-start(s16[272,128]{1,0:T(8,128)(2,1)S(1)} %get-tuple-element.45), channel_id=1, source_target_pairs={{0,6},{2,4},{4,2},{6,0},{1,7},{3,5},{5,3},{7,1},{8,14},{10,12},{12... | collective-permute-start | bytes 208904 | tf_op jit(solution)/shard_map/ppermute | solution.py:421
  43.2 0.5 collective-permute-start.18
  43.7 0.0 collective-permute-done.12.refs_5_.refs_13_
  43.7 0.0 collective-permute-done.11.refs_4_.refs_12_
  43.7 0.0 collective-permute-done.10.refs_3_.refs_11_
  43.7 0.8 %carries_1.1 = (s16[272,128]{1,0:T(8,128)(2,1)S(1)}, s16[272,128]{1,0:T(8,128)(2,1)S(1)}) custom-call(s32[4]{0:T(128)S(1)} %pad_add_fusion.place_ref, f32[2,128,128]{2,1,0:T(8,128)S(1)} %get-tuple-element.34.refs_3_.own_ref.refs_7_, s16[272,128]{1,0:T(8,128)(2,1)S(1)} %collective-permute-done.4.refs_0_.refs_8_, ...), custom_call_target="tpu_custom_call" | custom-call | bytes 1245184 | tf_op jit(solution)/shard_map/carries_1/pallas_call | solution.py:254
  44.5 1.6 %collective-permute-start.17 = (s16[272,128]{1,0:T(8,128)(2,1)S(1)}, s16[272,128]{1,0:T(8,128)(2,1)S(1)}, u32[]{:S(2)}, u32[]{:S(2)}) collective-permute-start(s16[272,128]{1,0:T(8,128)(2,1)S(1)} %get-tuple-element.43), channel_id=1, source_target_pairs={{0,6},{2,4},{4,2},{6,0},{1,7},{3,5},{5,3},{7,1},{8,14},{10,12},{12... | collective-permute-start | bytes 208904 | tf_op jit(solution)/shard_map/ppermute | solution.py:421
  46.1 1.2 %collective-permute-start.16 = (s16[272,128]{1,0:T(8,128)(2,1)S(1)}, s16[272,128]{1,0:T(8,128)(2,1)S(1)}, u32[]{:S(2)}, u32[]{:S(2)}) collective-permute-start(s16[272,128]{1,0:T(8,128)(2,1)S(1)} %get-tuple-element.42.refs_2_), channel_id=1, source_target_pairs={{0,2},{2,0},{4,6},{6,4},{1,3},{3,1},{5,7},{7,5},{8,10},{10,8},{12,... | collective-permute-start | bytes 208904 | tf_op jit(solution)/shard_map/ppermute | solution.py:421
  47.2 0.0 collective-permute-done.19.refs_1_
  47.2 1.1 %collective-permute-done.18.refs_0_ = s16[272,128]{1,0:T(8,128)(2,1)S(1)} collective-permute-done((s16[272,128]{1,0:T(8,128)(2,1)S(1)}, s16[272,128]{1,0:T(8,128)(2,1)S(1)}, u32[]{:S(2)}, u32[]{:S(2)}) %collective-permute-start.18) | collective-permute-done | bytes 69664 | tf_op jit(solution)/shard_map/ppermute | solution.py:421
  48.4 1.9 %attend_0_1_3.1.refs_2_ = bf16[512,512]{1,0:T(8,128)(2,1)S(1)} custom-call(s32[4]{0:T(128)S(1)} %pad_add_fusion.place_ref, bf16[256,2048]{1,0:T(8,128)(2,1)S(1)} %copy-done.2, bf16[256,2048]{1,0:T(8,128)(2,1)S(1)} %collective-permute-done.refs_1_.q_sib_ref, bf16[256,2048]{1,0:T(8,128)(2,1)S(1)} %get-tuple-element.28.k_ref, ...), custom_call_target="tpu_custom_call" | custom-call | flops 402653184 | bytes 2097152 | tf_op jit(solution)/shard_map/attend_0_1_3/pallas_call | solution.py:346
  50.3 1.2 %collective-permute-start.22 = (bf16[512,512]{1,0:T(8,128)(2,1)S(1)}, bf16[512,512]{1,0:T(8,128)(2,1)S(1)}, u32[]{:S(2)}, u32[]{:S(2)}) collective-permute-start(bf16[512,512]{1,0:T(8,128)(2,1)S(1)} %attend_0_1_3.1.refs_2_), channel_id=1, source_target_pairs={{0,2},{2,0},{1,3},{3,1},{4,6},{6,4},{5,7},{7,5},{8,10},{10,8},{9,1... | collective-permute-start | bytes 1572872 | tf_op jit(solution)/shard_map/ppermute | solution.py:421
  51.5 0.0 collective-permute-done.17.refs_1_
  51.5 0.0 collective-permute-done.16.refs_0_
  51.5 1.9 %attend_1_1_3.1.refs_14_.refs_2_ = bf16[512,512]{1,0:T(8,128)(2,1)S(1)} custom-call(s32[4]{0:T(128)S(1)} %pad_add_fusion.place_ref, bf16[256,2048]{1,0:T(8,128)(2,1)S(1)} %copy-done.2, bf16[256,2048]{1,0:T(8,128)(2,1)S(1)} %collective-permute-done.refs_1_.q_sib_ref, bf16[256,2048]{1,0:T(8,128)(2,1)S(1)} %get-tuple-element.28.k_ref, ...), custom_call_target="tpu_custom_call" | custom-call | flops 402653184 | bytes 2097152 | tf_op jit(solution)/shard_map/attend_1_1_3/pallas_call | solution.py:346
  53.4 1.5 %collective-permute-start.20 = (bf16[512,512]{1,0:T(8,128)(2,1)S(1)}, bf16[512,512]{1,0:T(8,128)(2,1)S(1)}, u32[]{:S(2)}, u32[]{:S(2)}) collective-permute-start(bf16[512,512]{1,0:T(8,128)(2,1)S(1)} %attend_1_1_3.1.refs_14_.refs_2_), channel_id=1, source_target_pairs={{0,2},{2,0},{1,3},{3,1},{4,6},{6,4},{5,7},{7,5},{8,10},{10,8},{9,1... | collective-permute-start | bytes 1572872 | tf_op jit(solution)/shard_map/ppermute | solution.py:421
  54.8 1.1 %own_carries.1 = (s16[528,128]{1,0:T(8,128)(2,1)S(1)}, s16[528,128]{1,0:T(8,128)(2,1)S(1)}, f32[2,2,128,128]{3,2,1,0:T(8,128)S(1)}, f32[2,2,128,128]{3,2,1,0:T(8,128)S(1)}) custom-call(s32[4]{0:T(128)S(1)} %pad_add_fusion.place_ref, f32[2,128,128]{2,1,0:T(8,128)S(1)} %get-tuple-element.32.refs_0_.own_ref, ...), custom_call_target="tpu_custom_call" | custom-call | bytes 2490368 | tf_op jit(solution)/shard_map/own_carries/pallas_call | solution.py:288
  56.0 0.6 collective-permute-start.23
  56.5 1.5 %collective-permute-start.21 = (s16[528,128]{1,0:T(8,128)(2,1)S(1)}, s16[528,128]{1,0:T(8,128)(2,1)S(1)}, u32[]{:S(2)}, u32[]{:S(2)}) collective-permute-start(s16[528,128]{1,0:T(8,128)(2,1)S(1)} %get-tuple-element.47), channel_id=1, source_target_pairs={{0,4},{2,6},{4,0},{6,2},{1,5},{3,7},{5,1},{7,3},{8,12},{10,14},{12... | collective-permute-start | bytes 405512 | tf_op jit(solution)/shard_map/ppermute | solution.py:421
  58.1 5.8 %collective-permute-done.21.refs_1_ = s16[528,128]{1,0:T(8,128)(2,1)S(1)} collective-permute-done((s16[528,128]{1,0:T(8,128)(2,1)S(1)}, s16[528,128]{1,0:T(8,128)(2,1)S(1)}, u32[]{:S(2)}, u32[]{:S(2)}) %collective-permute-start.21) | collective-permute-done | bytes 135200 | tf_op jit(solution)/shard_map/ppermute | solution.py:421
  63.9 1.9 %attend_0_0_2.1.refs_2_.refs_0_ = bf16[512,512]{1,0:T(8,128)(2,1)S(1)} custom-call(s32[4]{0:T(128)S(1)} %pad_add_fusion.place_ref, bf16[256,2048]{1,0:T(8,128)(2,1)S(1)} %copy-done.2, bf16[256,2048]{1,0:T(8,128)(2,1)S(1)} %collective-permute-done.refs_1_.q_sib_ref, bf16[256,2048]{1,0:T(8,128)(2,1)S(1)} %get-tuple-element.28.k_ref, ...), custom_call_target="tpu_custom_call" | custom-call | flops 402653184 | bytes 2097152 | tf_op jit(solution)/shard_map/attend_0_0_2/pallas_call | solution.py:346
  65.7 1.9 %attend_1_0_2.1.refs_1_ = bf16[512,512]{1,0:T(8,128)(2,1)S(1)} custom-call(s32[4]{0:T(128)S(1)} %pad_add_fusion.place_ref, bf16[256,2048]{1,0:T(8,128)(2,1)S(1)} %copy-done.2, bf16[256,2048]{1,0:T(8,128)(2,1)S(1)} %collective-permute-done.refs_1_.q_sib_ref, bf16[256,2048]{1,0:T(8,128)(2,1)S(1)} %get-tuple-element.28.k_ref, ...), custom_call_target="tpu_custom_call" | custom-call | flops 402653184 | bytes 2097152 | tf_op jit(solution)/shard_map/attend_1_0_2/pallas_call | solution.py:346
  67.6 0.0 collective-permute-done.23.refs_1_
  67.6 1.4 %assemble_cache.1 = f32[1,8,128,128]{3,2,1,0:T(8,128)} custom-call(s32[4]{0:T(128)S(1)} %pad_add_fusion.place_ref, f32[2,2,128,128]{3,2,1,0:T(8,128)S(1)} %get-tuple-element.48.refs_0_, f32[2,2,128,128]{3,2,1,0:T(8,128)S(1)} %collective-permute-done.23.refs_1_), custom_call_target="tpu_custom_call" | custom-call | tf_op jit(solution)/shard_map/assemble_cache/pallas_call | solution.py:406
  69.0 1.7 %assemble.1.refs_1_ = bf16[1024,1024]{1,0:T(8,128)(2,1)} custom-call(s32[4]{0:T(128)S(1)} %pad_add_fusion.place_ref, bf16[512,512]{1,0:T(8,128)(2,1)S(1)} %attend_0_0_2.1.refs_2_.refs_0_, bf16[512,512]{1,0:T(8,128)(2,1)S(1)} %attend_1_0_2.1.refs_1_, bf16[512,512]{1,0:T(8,128)(2,1)S(1)} %collective-permute-done.22.refs_2_), custom_call_target="tpu_custom_call" | custom-call | tf_op jit(solution)/shard_map/assemble/pallas_call | solution.py:385
  70.7 1.8 %collective-permute-done.20.refs_0_ = bf16[512,512]{1,0:T(8,128)(2,1)S(1)} collective-permute-done((bf16[512,512]{1,0:T(8,128)(2,1)S(1)}, bf16[512,512]{1,0:T(8,128)(2,1)S(1)}, u32[]{:S(2)}, u32[]{:S(2)}) %collective-permute-start.20) | collective-permute-done | bytes 524320 | tf_op jit(solution)/shard_map/ppermute | solution.py:421
  72.5 1.4 %finish.1 = bf16[1024,1024]{1,0:T(8,128)(2,1)} custom-call(s32[4]{0:T(128)S(1)} %pad_add_fusion.place_ref, bf16[512,512]{1,0:T(8,128)(2,1)S(1)} %collective-permute-done.20.refs_0_, bf16[1024,1024]{1,0:T(8,128)(2,1)} %assemble.1.refs_1_), custom_call_target="tpu_custom_call", output_to_operand_aliasing={{}: (2, {})} | custom-call | tf_op jit(solution)/shard_map/finish/pallas_call | solution.py:385
  (8 shorter events, 0.0 us)
Async XLA Ops:
  0.7 8.3 %copy-start.3 = (f32[1024]{0:T(1024)S(1)}, f32[1024]{0:T(1024)}, u32[]{:S(2)}) copy-start(f32[1024]{0:T(1024)} %param.9) | copy-start | bytes 12292
  8.0 5.2 %collective-permute-start = (bf16[256,2048]{1,0:T(8,128)(2,1)}, bf16[256,2048]{1,0:T(8,128)(2,1)S(1)}, u32[]{:S(2)}, u32[]{:S(2)}) collective-permute-start(bf16[256,2048]{1,0:T(8,128)(2,1)} %get-tuple-element.27), channel_id=1, source_target_pairs={{0,1},{1,0},{2,3},{3,2},{4,5},{5,4},{6,7},{7,6},{8,9},{9,8},{10,11... | collective-permute-start | bytes 3145736 | tf_op jit(solution)/shard_map/ppermute | solution.py:421
  8.5 4.7 %collective-permute-start.1 = (bf16[256,2048]{1,0:T(8,128)(2,1)}, bf16[256,2048]{1,0:T(8,128)(2,1)S(1)}, u32[]{:S(2)}, u32[]{:S(2)}) collective-permute-start(bf16[256,2048]{1,0:T(8,128)(2,1)} %get-tuple-element.29), channel_id=1, source_target_pairs={{0,1},{1,0},{2,3},{3,2},{4,5},{5,4},{6,7},{7,6},{8,9},{9,8},{10,11... | collective-permute-start | bytes 3145736 | tf_op jit(solution)/shard_map/ppermute | solution.py:421
  8.6 5.4 %collective-permute-start.2 = (bf16[256,2048]{1,0:T(8,128)(2,1)}, bf16[256,2048]{1,0:T(8,128)(2,1)S(1)}, u32[]{:S(2)}, u32[]{:S(2)}) collective-permute-start(bf16[256,2048]{1,0:T(8,128)(2,1)} %get-tuple-element.31), channel_id=1, source_target_pairs={{0,1},{1,0},{2,3},{3,2},{4,5},{5,4},{6,7},{7,6},{8,9},{9,8},{10,11... | collective-permute-start | bytes 3145736 | tf_op jit(solution)/shard_map/ppermute | solution.py:421
  9.0 4.2 %collective-permute-start.3 = (f32[1,1024]{1,0:T(1,128)S(1)}, f32[1,1024]{1,0:T(1,128)S(1)}, u32[]{:S(2)}, u32[]{:S(2)}) collective-permute-start(f32[1,1024]{1,0:T(1,128)S(1)} %bitcast.5), channel_id=1, source_target_pairs={{0,2},{2,0},{1,3},{3,1},{4,6},{6,4},{5,7},{7,5},{8,10},{10,8},{9,1... | collective-permute-start | bytes 12296 | tf_op jit(solution)/shard_map/ppermute | solution.py:421
  14.0 1.2 %copy-start = (bf16[256,2048]{1,0:T(8,128)(2,1)S(1)}, bf16[256,2048]{1,0:T(8,128)(2,1)}, u32[]{:S(2)}) copy-start(bf16[256,2048]{1,0:T(8,128)(2,1)} %get-tuple-element.30.v_ref) | copy-start | bytes 3145732
  16.6 9.4 %collective-permute-start.7 = (s16[272,128]{1,0:T(8,128)(2,1)S(1)}, s16[272,128]{1,0:T(8,128)(2,1)S(1)}, u32[]{:S(2)}, u32[]{:S(2)}) collective-permute-start(s16[272,128]{1,0:T(8,128)(2,1)S(1)} %get-tuple-element.38), channel_id=1, source_target_pairs={{0,2},{2,0},{4,6},{6,4},{1,3},{3,1},{5,7},{7,5},{8,10},{10,8},{12,... | collective-permute-start | bytes 208904 | tf_op jit(solution)/shard_map/ppermute | solution.py:421
  19.5 6.5 %collective-permute-start.8 = (s16[272,128]{1,0:T(8,128)(2,1)S(1)}, s16[272,128]{1,0:T(8,128)(2,1)S(1)}, u32[]{:S(2)}, u32[]{:S(2)}) collective-permute-start(s16[272,128]{1,0:T(8,128)(2,1)S(1)} %get-tuple-element.39), channel_id=1, source_target_pairs={{0,4},{2,6},{4,0},{6,2},{1,5},{3,7},{5,1},{7,3},{8,12},{10,14},{12... | collective-permute-start | bytes 208904 | tf_op jit(solution)/shard_map/ppermute | solution.py:421
  21.0 5.6 %collective-permute-start.9 = (s16[272,128]{1,0:T(8,128)(2,1)S(1)}, s16[272,128]{1,0:T(8,128)(2,1)S(1)}, u32[]{:S(2)}, u32[]{:S(2)}) collective-permute-start(s16[272,128]{1,0:T(8,128)(2,1)S(1)} %get-tuple-element.40), channel_id=1, source_target_pairs={{0,6},{2,4},{4,2},{6,0},{1,7},{3,5},{5,3},{7,1},{8,14},{10,12},{12... | collective-permute-start | bytes 208904 | tf_op jit(solution)/shard_map/ppermute | solution.py:421
  22.5 25.9 %copy-start.1 = (bf16[256,2048]{1,0:T(8,128)(2,1)S(1)}, bf16[256,2048]{1,0:T(8,128)(2,1)}, u32[]{:S(2)}) copy-start(bf16[256,2048]{1,0:T(8,128)(2,1)} %get-tuple-element.30.v_ref) | copy-start | bytes 3145732
  22.5 25.9 %copy-start.2 = (bf16[256,2048]{1,0:T(8,128)(2,1)S(1)}, bf16[256,2048]{1,0:T(8,128)(2,1)}, u32[]{:S(2)}) copy-start(bf16[256,2048]{1,0:T(8,128)(2,1)} %get-tuple-element.26.q_ref) | copy-start | bytes 3145732
  22.5 12.1 %collective-permute-start.4 = (s16[272,128]{1,0:T(8,128)(2,1)S(1)}, s16[272,128]{1,0:T(8,128)(2,1)S(1)}, u32[]{:S(2)}, u32[]{:S(2)}) collective-permute-start(s16[272,128]{1,0:T(8,128)(2,1)S(1)} %get-tuple-element.35), channel_id=1, source_target_pairs={{0,2},{2,0},{4,6},{6,4},{1,3},{3,1},{5,7},{7,5},{8,10},{10,8},{12,... | collective-permute-start | bytes 208904 | tf_op jit(solution)/shard_map/ppermute | solution.py:421
  24.5 11.4 %collective-permute-start.5 = (s16[272,128]{1,0:T(8,128)(2,1)S(1)}, s16[272,128]{1,0:T(8,128)(2,1)S(1)}, u32[]{:S(2)}, u32[]{:S(2)}) collective-permute-start(s16[272,128]{1,0:T(8,128)(2,1)S(1)} %get-tuple-element.36), channel_id=1, source_target_pairs={{0,4},{2,6},{4,0},{6,2},{1,5},{3,7},{5,1},{7,3},{8,12},{10,14},{12... | collective-permute-start | bytes 208904 | tf_op jit(solution)/shard_map/ppermute | solution.py:421
  26.0 10.0 %collective-permute-start.6 = (s16[272,128]{1,0:T(8,128)(2,1)S(1)}, s16[272,128]{1,0:T(8,128)(2,1)S(1)}, u32[]{:S(2)}, u32[]{:S(2)}) collective-permute-start(s16[272,128]{1,0:T(8,128)(2,1)S(1)} %get-tuple-element.37), channel_id=1, source_target_pairs={{0,6},{2,4},{4,2},{6,0},{1,7},{3,5},{5,3},{7,1},{8,14},{10,12},{12... | collective-permute-start | bytes 208904 | tf_op jit(solution)/shard_map/ppermute | solution.py:421
  26.8 12.5 %collective-permute-start.15 = (s16[272,128]{1,0:T(8,128)(2,1)S(1)}, s16[272,128]{1,0:T(8,128)(2,1)S(1)}, u32[]{:S(2)}, u32[]{:S(2)}) collective-permute-start(s16[272,128]{1,0:T(8,128)(2,1)S(1)} %level_states_0.1.refs_3_), channel_id=1, source_target_pairs={{0,8},{8,16},{16,24},{1,9},{9,17},{17,25},{2,10},{10,18},{18,26},{... | collective-permute-start | bytes 208904 | tf_op jit(solution)/shard_map/ppermute | solution.py:428
  30.1 10.5 %collective-permute-start.14 = (s16[272,128]{1,0:T(8,128)(2,1)S(1)}, s16[272,128]{1,0:T(8,128)(2,1)S(1)}, u32[]{:S(2)}, u32[]{:S(2)}) collective-permute-start(s16[272,128]{1,0:T(8,128)(2,1)S(1)} %level_states_0.1.refs_3_), channel_id=1, source_target_pairs={{0,16},{8,24},{1,17},{9,25},{2,18},{10,26},{3,19},{11,27},{4,20},{... | collective-permute-start | bytes 208904 | tf_op jit(solution)/shard_map/ppermute | solution.py:428
  34.6 6.0 %collective-permute-start.13 = (s16[272,128]{1,0:T(8,128)(2,1)S(1)}, s16[272,128]{1,0:T(8,128)(2,1)S(1)}, u32[]{:S(2)}, u32[]{:S(2)}) collective-permute-start(s16[272,128]{1,0:T(8,128)(2,1)S(1)} %level_states_0.1.refs_3_), channel_id=1, source_target_pairs={{0,24},{1,25},{2,26},{3,27},{4,28},{5,29},{6,30},{7,31}} | collective-permute-start | bytes 208904 | tf_op jit(solution)/shard_map/ppermute | solution.py:428
  36.1 7.7 %collective-permute-start.12 = (s16[272,128]{1,0:T(8,128)(2,1)S(1)}, s16[272,128]{1,0:T(8,128)(2,1)S(1)}, u32[]{:S(2)}, u32[]{:S(2)}) collective-permute-start(s16[272,128]{1,0:T(8,128)(2,1)S(1)} %level_states_1.1.refs_6_), channel_id=1, source_target_pairs={{0,8},{8,16},{16,24},{1,9},{9,17},{17,25},{2,10},{10,18},{18,26},{... | collective-permute-start | bytes 208904 | tf_op jit(solution)/shard_map/ppermute | solution.py:428
  37.4 6.4 %collective-permute-start.11 = (s16[272,128]{1,0:T(8,128)(2,1)S(1)}, s16[272,128]{1,0:T(8,128)(2,1)S(1)}, u32[]{:S(2)}, u32[]{:S(2)}) collective-permute-start(s16[272,128]{1,0:T(8,128)(2,1)S(1)} %level_states_1.1.refs_6_), channel_id=1, source_target_pairs={{0,16},{8,24},{1,17},{9,25},{2,18},{10,26},{3,19},{11,27},{4,20},{... | collective-permute-start | bytes 208904 | tf_op jit(solution)/shard_map/ppermute | solution.py:428
  39.3 4.4 %collective-permute-start.10 = (s16[272,128]{1,0:T(8,128)(2,1)S(1)}, s16[272,128]{1,0:T(8,128)(2,1)S(1)}, u32[]{:S(2)}, u32[]{:S(2)}) collective-permute-start(s16[272,128]{1,0:T(8,128)(2,1)S(1)} %level_states_1.1.refs_6_), channel_id=1, source_target_pairs={{0,24},{1,25},{2,26},{3,27},{4,28},{5,29},{6,30},{7,31}} | collective-permute-start | bytes 208904 | tf_op jit(solution)/shard_map/ppermute | solution.py:428
  41.4 5.9 %collective-permute-start.19 = (s16[272,128]{1,0:T(8,128)(2,1)S(1)}, s16[272,128]{1,0:T(8,128)(2,1)S(1)}, u32[]{:S(2)}, u32[]{:S(2)}) collective-permute-start(s16[272,128]{1,0:T(8,128)(2,1)S(1)} %get-tuple-element.45), channel_id=1, source_target_pairs={{0,6},{2,4},{4,2},{6,0},{1,7},{3,5},{5,3},{7,1},{8,14},{10,12},{12... | collective-permute-start | bytes 208904 | tf_op jit(solution)/shard_map/ppermute | solution.py:421
  43.2 5.2 %collective-permute-start.18 = (s16[272,128]{1,0:T(8,128)(2,1)S(1)}, s16[272,128]{1,0:T(8,128)(2,1)S(1)}, u32[]{:S(2)}, u32[]{:S(2)}) collective-permute-start(s16[272,128]{1,0:T(8,128)(2,1)S(1)} %get-tuple-element.41.refs_6_), channel_id=1, source_target_pairs={{0,2},{2,0},{4,6},{6,4},{1,3},{3,1},{5,7},{7,5},{8,10},{10,8},{12,... | collective-permute-start | bytes 208904 | tf_op jit(solution)/shard_map/ppermute | solution.py:421
  44.5 7.0 %collective-permute-start.17 = (s16[272,128]{1,0:T(8,128)(2,1)S(1)}, s16[272,128]{1,0:T(8,128)(2,1)S(1)}, u32[]{:S(2)}, u32[]{:S(2)}) collective-permute-start(s16[272,128]{1,0:T(8,128)(2,1)S(1)} %get-tuple-element.43), channel_id=1, source_target_pairs={{0,6},{2,4},{4,2},{6,0},{1,7},{3,5},{5,3},{7,1},{8,14},{10,12},{12... | collective-permute-start | bytes 208904 | tf_op jit(solution)/shard_map/ppermute | solution.py:421
  46.1 5.4 %collective-permute-start.16 = (s16[272,128]{1,0:T(8,128)(2,1)S(1)}, s16[272,128]{1,0:T(8,128)(2,1)S(1)}, u32[]{:S(2)}, u32[]{:S(2)}) collective-permute-start(s16[272,128]{1,0:T(8,128)(2,1)S(1)} %get-tuple-element.42.refs_2_), channel_id=1, source_target_pairs={{0,2},{2,0},{4,6},{6,4},{1,3},{3,1},{5,7},{7,5},{8,10},{10,8},{12,... | collective-permute-start | bytes 208904 | tf_op jit(solution)/shard_map/ppermute | solution.py:421
  50.3 18.7 %collective-permute-start.22 = (bf16[512,512]{1,0:T(8,128)(2,1)S(1)}, bf16[512,512]{1,0:T(8,128)(2,1)S(1)}, u32[]{:S(2)}, u32[]{:S(2)}) collective-permute-start(bf16[512,512]{1,0:T(8,128)(2,1)S(1)} %attend_0_1_3.1.refs_2_), channel_id=1, source_target_pairs={{0,2},{2,0},{1,3},{3,1},{4,6},{6,4},{5,7},{7,5},{8,10},{10,8},{9,1... | collective-permute-start | bytes 1572872 | tf_op jit(solution)/shard_map/ppermute | solution.py:421
  53.4 19.1 %collective-permute-start.20 = (bf16[512,512]{1,0:T(8,128)(2,1)S(1)}, bf16[512,512]{1,0:T(8,128)(2,1)S(1)}, u32[]{:S(2)}, u32[]{:S(2)}) collective-permute-start(bf16[512,512]{1,0:T(8,128)(2,1)S(1)} %attend_1_1_3.1.refs_14_.refs_2_), channel_id=1, source_target_pairs={{0,2},{2,0},{1,3},{3,1},{4,6},{6,4},{5,7},{7,5},{8,10},{10,8},{9,1... | collective-permute-start | bytes 1572872 | tf_op jit(solution)/shard_map/ppermute | solution.py:421
  56.0 11.6 %collective-permute-start.23 = (f32[2,2,128,128]{3,2,1,0:T(8,128)S(1)}, f32[2,2,128,128]{3,2,1,0:T(8,128)S(1)}, u32[]{:S(2)}, u32[]{:S(2)}) collective-permute-start(f32[2,2,128,128]{3,2,1,0:T(8,128)S(1)} %get-tuple-element.49), channel_id=1, source_target_pairs={{0,4},{4,0},{1,5},{5,1},{2,6},{6,2},{3,7},{7,3},{8,12},{12,8},{9,1... | collective-permute-start | bytes 786440 | tf_op jit(solution)/shard_map/ppermute | solution.py:421
  56.5 7.3 %collective-permute-start.21 = (s16[528,128]{1,0:T(8,128)(2,1)S(1)}, s16[528,128]{1,0:T(8,128)(2,1)S(1)}, u32[]{:S(2)}, u32[]{:S(2)}) collective-permute-start(s16[528,128]{1,0:T(8,128)(2,1)S(1)} %get-tuple-element.47), channel_id=1, source_target_pairs={{0,4},{2,6},{4,0},{6,2},{1,5},{3,7},{5,1},{7,3},{8,12},{10,14},{12... | collective-permute-start | bytes 405512 | tf_op jit(solution)/shard_map/ppermute | solution.py:421

commit v5 on v4

--- a/solution.py
+++ b/solution.py
@@ -12,7 +12,7 @@
 SCORE_SCALE = HD ** (-0.5)
 CORES = 2
 VMEM_BYTES = 24 * 1024 * 1024
-DECODE_VMEM_BYTES = 52 * 1024 * 1024
+DECODE_VMEM_BYTES = 46 * 1024 * 1024
 PAD = 16
 TOP = 32767.0
 
@@ -46,33 +46,34 @@
         self.piece = self.each * HD
 
 
-def counts_of(spikes, names):
+def counts_of(spikes):
     one, two = jnp.ones_like(spikes), jnp.full_like(spikes, 2)
     zero = jnp.zeros_like(spikes)
 
     def ternary(rest, unit):
         return jnp.where(rest >= 2 * unit, two, jnp.where(rest >= unit, one, zero))
 
-    counts = {"value": ternary(spikes, 9)}
-    if names != ("value",):
-        rest = spikes - 9 * counts["value"]
-        counts["key"] = ternary(rest, 3)
-        if "query" in names:
-            counts["query"] = rest - 3 * counts["key"]
-    return counts
-
-
-def decode(plan, place, spikes, operands):
-    names = tuple(operands)
+    value = ternary(spikes, 9)
+    rest = spikes - 9 * value
+    key = ternary(rest, 3)
+    return value, key, rest - 3 * key
+
+
+def sides(plan, place_ref):
+    for y in range(plan.n_y):
+        for side in range(CORES):
+            of = place_ref[0] if side == 0 else 1 - place_ref[0]
+            start = pl.multiple_of((y * CORES + of) * plan.width, plan.width)
+            yield side, slice(y * plan.width, (y + 1) * plan.width), pl.ds(start, plan.width)
+
+
+def decode(plan, place, spikes, keys, values):
     rows, model = spikes.shape
     step = min(rows, 32)
     chunks = rows // step
-    width = plan.width
-    n = len(names)
 
     def kernel(place_ref, *refs):
-        sources, outs = refs[: 1 + n], refs[1 + n : 1 + 3 * n]
-        buffers, sems = refs[1 + 3 * n : -1], refs[-1]
+        sources, outs, buffers, sems = refs[:3], refs[3:9], refs[9:12], refs[12]
 
         def fetch(chunk, index):
             at = pl.ds(chunk * step, step)
@@ -81,37 +82,52 @@
             )
 
         for chunk in range(chunks):
-            for index in range(1 + n):
+            for index in range(3):
                 fetch(chunk, index).start()
 
         @pl.loop(0, chunks)
         def _(chunk):
-            for index in range(1 + n):
+            for index in range(3):
                 fetch(chunk, index).wait()
             at = pl.ds(pl.multiple_of(chunk * step, step), step)
-            for y in range(plan.n_y):
-                for side in range(CORES):
-                    of = place_ref[0] if side == 0 else 1 - place_ref[0]
-                    columns = pl.ds(pl.multiple_of((y * CORES + of) * width, width), width)
-                    codes = buffers[0][at, columns].astype(jnp.float32).astype(jnp.bfloat16)
-                    counts = counts_of(codes, names)
-                    for index, name in enumerate(names):
-                        outs[2 * index + side][at, y * width : (y + 1) * width] = (
-                            buffers[1 + index][at, columns] * counts[name]
-                        )
-
-    return pl.pallas_call(
-        kernel,
-        out_shape=[jax.ShapeDtypeStruct((rows, plan.n_y * width), jnp.bfloat16)] * (2 * n),
-        in_specs=[SMEM] + [HBM] * (1 + n),
-        out_specs=[VMEM] * (2 * n),
-        scratch_shapes=[pltpu.VMEM((rows, model), jnp.int32)]
-        + [pltpu.VMEM((rows, model), jnp.bfloat16)] * n
-        + [pltpu.SemaphoreType.DMA((chunks, 1 + n))],
+            for side, mine, columns in sides(plan, place_ref):
+                spikes = buffers[0][at, columns].astype(jnp.float32).astype(jnp.bfloat16)
+                value, key, query = counts_of(spikes)
+                outs[side][at, mine] = buffers[1][at, columns] * key
+                outs[2 + side][at, mine] = buffers[2][at, columns] * value
+                outs[4 + side][at, mine] = query
+
+    return pl.pallas_call(
+        kernel,
+        out_shape=[jax.ShapeDtypeStruct((rows, plan.n_y * plan.width), jnp.bfloat16)] * 6,
+        in_specs=[SMEM] + [HBM] * 3,
+        out_specs=[VMEM] * 6,
+        scratch_shapes=[
+            pltpu.VMEM((rows, model), jnp.int32),
+            pltpu.VMEM((rows, model), jnp.bfloat16),
+            pltpu.VMEM((rows, model), jnp.bfloat16),
+            pltpu.SemaphoreType.DMA((chunks, 3)),
+        ],
         compiler_params=params(DECODE_VMEM_BYTES),
-        cost_estimate=cost(rows * model * 4, rows * model * (4 + 4 * n)),
+        cost_estimate=cost(rows * model * 4, rows * model * 14),
         name="decode",
-    )(place, spikes, *operands.values())
+    )(place, spikes, keys, values)
+
+
+def spike_queries(plan, place, queries, counts):
+    def kernel(place_ref, queries_ref, *refs):
+        for side, mine, columns in sides(plan, place_ref):
+            refs[2 + side][:, mine] = queries_ref[:, columns] * refs[side][:, mine]
+
+    return pl.pallas_call(
+        kernel,
+        out_shape=[jax.ShapeDtypeStruct(a.shape, jnp.bfloat16) for a in counts],
+        in_specs=[SMEM] + [VMEM] * 3,
+        out_specs=[VMEM] * 2,
+        compiler_params=params(),
+        cost_estimate=cost(queries.size, queries.size * 6),
+        name="spike_queries",
+    )(place, queries, *counts)
 
 
 def contract_rows(left, right):
@@ -429,24 +445,23 @@
 
     gain = gain.reshape(1, plan.width)
     gains = [gain] + [swap(gain, "y", o, plan.n_y) for o in range(1, plan.n_y)]
-    arrays = decode(plan, place, spikes, {"key": keys, "value": values, "query": queries})
-    key, value, query = (
-        (mine, swap(sibling, "core", 1, CORES)) for mine, sibling in zip(arrays[::2], arrays[1::2])
-    )
-
-    after = [*gains[1:], query[1]]
-    own, first, others = [], [], []
-    for half in halves:
+    key, key_out, value, value_out, *counts = decode(plan, place, spikes, keys, values)
+    key, value = ((a, swap(b, "core", 1, CORES)) for a, b in ((key, key_out), (value, value_out)))
+    query, query_out = spike_queries(plan, place, queries, counts)
+    query = (query, swap(query_out, "core", 1, CORES))
+
+    own, first, others, levels, coded = [], [], [], [], []
+
+    def owner_stage(half, after):
         mine, parts, *sends = chunk_states(plan, place, key, value, half, after)
         own.append(mine)
         first.append(parts)
         others.append([in_level(a, o) for o, a in enumerate(sends, 1)])
-        after = [mine]
-    levels = []
-    for half in halves:
+
+    def level_stage(half, after):
         level = level_states(plan, own[half], others[half], half, after)
+        coded.append(level)
         levels.append([to_later(level, d) for d in range(plan.n_outer - 1, 0, -1)])
-        after = [level]
 
     of_group = [list(range(y, plan.plane, plan.n_y)) for y in range(plan.n_y)]
     abroad = [o for offsets in of_group[1:] for o in offsets]
@@ -466,17 +481,34 @@
             after,
         )
 
-    carry = []
-    for half in halves:
+    def carry_stage(half, after):
         sends = carries(plan, place, own[half], others[half], levels[half], half, abroad, after)
-        carry.append({o: in_level(a, o) for o, a in zip(abroad, sends)})
-        after = [sends[0]]
+        return sends[0], {o: in_level(a, o) for o, a in zip(abroad, sends)}
+
     parts = []
-    for half in halves:
+
+    def send_stage(half, carry, after):
         for y in range(1, plan.n_y):
-            part = part_of(half, of_group[y], carry[half], after)
-            parts.append((swap(part, "y", y, plan.n_y), half, of_group[y]))
-            after = [part]
+            group = of_group[y]
+            pieces = [group[:-1], group[-1:]] if half and len(group) > 1 else [group]
+            for offsets in pieces:
+                arrived = [a for a, h, os in parts if h == 0 and offsets == group[-1:] and os == group]
+                part = part_of(half, offsets, carry, after + arrived)
+                parts.append((swap(part, "y", y, plan.n_y), half, offsets))
+                after = [part]
+        return after
+
+    owner_stage(0, [query[0]])
+    level_stage(0, gains[1:])
+    if plan.halves > 1:
+        owner_stage(1, [coded[0], query[1]])
+    done, carry = carry_stage(0, [own[-1]])
+    if plan.halves > 1:
+        level_stage(1, [done])
+    after = send_stage(0, carry, [coded[-1]])
+    if plan.halves > 1:
+        _, carry = carry_stage(1, after)
+        after = send_stage(1, carry, [])
     sends = own_carries(plan, place, own, others, levels, of_group[0], after)
     own_carry = {o: in_level(a, o) if o else a for o, a in zip(of_group[0], sends)}
     caches = [

time: 74.1 us -> 80.4 us (1.085)
  waiting for transfers between devices: 11.8 us -> 18.9 us
  starting transfers between devices: 35.2 us -> 37 us
  Pallas kernels: 24.8 us -> 23.4 us
  local copies, waits for them, and re-layouts: 1.24 us -> 0.01 us
    ppermute x18 -> x19, waiting for transfers between devices: 11.8 us -> 17 us  [swap(): return lax.ppermute(array, axes, [(i, i ^ offset) for i in range(size)])]
    pallas_call x1, Pallas kernels: 7.26 us -> 4.36 us  [decode(): pl.pallas_call(kernel, out_shape=[jax.ShapeDtypeStruct((rows, plan.n_y *...]
    ppermute x6, starting transfers between devices: 13.6 us -> 16.1 us  [to_later(): return lax.ppermute(array, 'outer', pairs)]
    ppermute x6, waiting for transfers between devices: 0.02 us -> 1.92 us  [to_later(): return lax.ppermute(array, 'outer', pairs)]
    unnamed x8 -> x4, local copies, waits for them, and re-layouts: 1.24 us -> 0.01 us
    pallas_call x4 -> x5, Pallas kernels: 7.49 us -> 8.28 us  [attend(): pl.pallas_call(kernel, out_shape=jax.ShapeDtypeStruct((CORES * rows, head...]
    ppermute x18 -> x19, starting transfers between devices: 21.5 us -> 20.9 us  [swap(): return lax.ppermute(array, axes, [(i, i ^ offset) for i in range(size)])]
  transfers between devices with their start and end apart: 24 -> 25, of which waited for: 6 -> 11; matrix products, arithmetic and copies ran while one was open for 0% -> 0% of each run, Pallas kernels for 20% -> 20%
where the time goes in v5:
time: 80.4 us; the launch traced here: 80.2 us
  starting transfers between devices  37 us (46%)
  Pallas kernels  23.4 us (29%)
  waiting for transfers between devices  18.9 us (24%)
  between operations  0.83 us (1%)
    ppermute x19, starting transfers between devices, swap(): return lax.ppermute(array, axes, [(i, i ^ offset) for i in range(size)])  20.9 us
    ppermute x19, waiting for transfers between devices, swap(): return lax.ppermute(array, axes, [(i, i ^ offset) for i in range(size)])  17 us
    ppermute x6, starting transfers between devices, to_later(): return lax.ppermute(array, 'outer', pairs)  16.1 us
    pallas_call x5, Pallas kernels, attend(): pl.pallas_call(kernel, out_shape=jax.ShapeDtypeStruct((CORES * rows, head...  8.28 us
    pallas_call x1, Pallas kernels, decode(): pl.pallas_call(kernel, out_shape=[jax.ShapeDtypeStruct((rows, plan.n_y *...  4.36 us
    pallas_call x2, Pallas kernels, assemble(): pl.pallas_call(kernel, out_shape=jax.ShapeDtypeStruct((plan.n_y * rows, p...  3.08 us
    pallas_call x2, Pallas kernels, chunk_states(): pl.pallas_call(kernel, out_shape=[states_shape(plan.each), states_shape(p...  2.73 us
    ppermute x6, waiting for transfers between devices, to_later(): return lax.ppermute(array, 'outer', pairs)  1.92 us
  transfers between devices with their start and end apart: 25, of which 11 were waited for; matrix products, arithmetic and copies ran while one was open for 0% of the time, Pallas kernels for 20%

profile of v5, /device:TPU:0, one launch (start us, length us, event | category | flops | bytes accessed | tf_op | source)
XLA Modules:
  0.0 80.2 jit_solution(2987084154694671371)
XLA Ops:
  0.6 0.1 pad_add_fusion.place_ref
  0.7 4.4 %decode.1 = (bf16[256,2048]{1,0:T(8,128)(2,1)S(1)}, bf16[256,2048]{1,0:T(8,128)(2,1)S(1)}, bf16[256,2048]{1,0:T(8,128)(2,1)S(1)}, bf16[256,2048]{1,0:T(8,128)(2,...) custom-call(s32[4]{0:T(128)S(1)} %pad_add_fusion.place_ref, s32[256,4096]{1,0:T(8,128)} %refs_0_.1, ...), custom_call_target="tpu_custom_call" | custom-call | flops 4194304 | bytes 14680064 | tf_op jit(solution)/shard_map/decode/pallas_call | solution.py:100
  5.1 0.5 collective-permute-start.1
  5.6 0.1 collective-permute-start.2
  5.7 0.8 spike_queries.1
  6.4 0.5 collective-permute-start
  6.9 0.9 %collective-permute-done.1.k_sib_ref = bf16[256,2048]{1,0:T(8,128)(2,1)S(1)} collective-permute-done((bf16[256,2048]{1,0:T(8,128)(2,1)S(1)}, bf16[256,2048]{1,0:T(8,128)(2,1)S(1)}, u32[]{:S(2)}, u32[]{:S(2)}) %collective-permute-start.1) | collective-permute-done | bytes 1048608 | tf_op jit(solution)/shard_map/ppermute | solution.py:437
  7.9 1.5 %collective-permute-done.2.v_sib_ref = bf16[256,2048]{1,0:T(8,128)(2,1)S(1)} collective-permute-done((bf16[256,2048]{1,0:T(8,128)(2,1)S(1)}, bf16[256,2048]{1,0:T(8,128)(2,1)S(1)}, u32[]{:S(2)}, u32[]{:S(2)}) %collective-permute-start.2) | collective-permute-done | bytes 1048608 | tf_op jit(solution)/shard_map/ppermute | solution.py:437
  9.4 1.4 %chunk_states_0.1 = (f32[2,128,128]{2,1,0:T(8,128)S(1)}, f32[4,2,128,128]{3,2,1,0:T(8,128)S(1)}, s16[272,128]{1,0:T(8,128)(2,1)S(1)}, s16[272,128]{1,0:T(8,128)(2,1)S(1)}, s16[272,128]{1,0:T(8,128)(2,1)S(1)}) custom-call(s32[4]{0:T(128)S(1)} %pad_add_fusion.place_ref, bf16[256,2048]{1,0:T(8,128)(2,1)S(1)} %get-tuple-element.32.k_ref, ...), custom_call_target="tpu_custom_call" | custom-call | flops 134217728 | bytes 2883584 | tf_op jit(solution)/shard_map/chunk_states_0/pallas_call | solution.py:206
  10.8 3.0 %collective-permute-start.3 = (s16[272,128]{1,0:T(8,128)(2,1)S(1)}, s16[272,128]{1,0:T(8,128)(2,1)S(1)}, u32[]{:S(2)}, u32[]{:S(2)}) collective-permute-start(s16[272,128]{1,0:T(8,128)(2,1)S(1)} %get-tuple-element.37), channel_id=1, source_target_pairs={{0,2},{2,0},{4,6},{6,4},{1,3},{3,1},{5,7},{7,5},{8,10},{10,8},{12,... | collective-permute-start | bytes 208904 | tf_op jit(solution)/shard_map/ppermute | solution.py:437
  13.7 1.5 %collective-permute-start.4 = (s16[272,128]{1,0:T(8,128)(2,1)S(1)}, s16[272,128]{1,0:T(8,128)(2,1)S(1)}, u32[]{:S(2)}, u32[]{:S(2)}) collective-permute-start(s16[272,128]{1,0:T(8,128)(2,1)S(1)} %get-tuple-element.38), channel_id=1, source_target_pairs={{0,4},{2,6},{4,0},{6,2},{1,5},{3,7},{5,1},{7,3},{8,12},{10,14},{12... | collective-permute-start | bytes 208904 | tf_op jit(solution)/shard_map/ppermute | solution.py:437
  15.2 0.0 collective-permute-start.5
  15.3 1.9 %collective-permute-start.6 = (f32[1,1024]{1,0:T(1,128)S(1)}, f32[1,1024]{1,0:T(1,128)S(1)}, u32[]{:S(2)}, u32[]{:S(2)}) collective-permute-start(f32[1,1024]{1,0:T(1,128)S(1)} %bitcast.5), channel_id=1, source_target_pairs={{0,2},{2,0},{1,3},{3,1},{4,6},{6,4},{5,7},{7,5},{8,10},{10,8},{9,1... | collective-permute-start | bytes 12296 | tf_op jit(solution)/shard_map/ppermute | solution.py:437
  17.2 1.9 %collective-permute-done.6.refs_3_.gain_ref = f32[1,1024]{1,0:T(1,128)S(1)} collective-permute-done((f32[1,1024]{1,0:T(1,128)S(1)}, f32[1,1024]{1,0:T(1,128)S(1)}, u32[]{:S(2)}, u32[]{:S(2)}) %collective-permute-start.6) | collective-permute-done | bytes 4128 | tf_op jit(solution)/shard_map/ppermute | solution.py:437
  19.1 0.0 collective-permute-done.3.refs_0_.refs_1_
  19.1 0.0 collective-permute-done.4.refs_1_.refs_2_
  19.1 1.3 %collective-permute-done.5.refs_2_.refs_3_ = s16[272,128]{1,0:T(8,128)(2,1)S(1)} collective-permute-done((s16[272,128]{1,0:T(8,128)(2,1)S(1)}, s16[272,128]{1,0:T(8,128)(2,1)S(1)}, u32[]{:S(2)}, u32[]{:S(2)}) %collective-permute-start.5) | collective-permute-done | bytes 69664 | tf_op jit(solution)/shard_map/ppermute | solution.py:437
  20.4 0.1 level_states_0.1.refs_0_
  20.5 3.5 %collective-permute-start.12 = (s16[272,128]{1,0:T(8,128)(2,1)S(1)}, s16[272,128]{1,0:T(8,128)(2,1)S(1)}, u32[]{:S(2)}, u32[]{:S(2)}) collective-permute-start(s16[272,128]{1,0:T(8,128)(2,1)S(1)} %level_states_0.1.refs_0_), channel_id=1, source_target_pairs={{0,8},{8,16},{16,24},{1,9},{9,17},{17,25},{2,10},{10,18},{18,26},{... | collective-permute-start | bytes 208904 | tf_op jit(solution)/shard_map/ppermute | solution.py:444
  24.0 4.5 %collective-permute-start.11 = (s16[272,128]{1,0:T(8,128)(2,1)S(1)}, s16[272,128]{1,0:T(8,128)(2,1)S(1)}, u32[]{:S(2)}, u32[]{:S(2)}) collective-permute-start(s16[272,128]{1,0:T(8,128)(2,1)S(1)} %level_states_0.1.refs_0_), channel_id=1, source_target_pairs={{0,16},{8,24},{1,17},{9,25},{2,18},{10,26},{3,19},{11,27},{4,20},{... | collective-permute-start | bytes 208904 | tf_op jit(solution)/shard_map/ppermute | solution.py:444
  28.5 1.3 %collective-permute-start.10 = (s16[272,128]{1,0:T(8,128)(2,1)S(1)}, s16[272,128]{1,0:T(8,128)(2,1)S(1)}, u32[]{:S(2)}, u32[]{:S(2)}) collective-permute-start(s16[272,128]{1,0:T(8,128)(2,1)S(1)} %level_states_0.1.refs_0_), channel_id=1, source_target_pairs={{0,24},{1,25},{2,26},{3,27},{4,28},{5,29},{6,30},{7,31}} | collective-permute-start | bytes 208904 | tf_op jit(solution)/shard_map/ppermute | solution.py:444
  29.8 0.0 collective-permute-done.refs_1_.q_sib_ref
  29.8 1.4 %chunk_states_1.1 = (f32[2,128,128]{2,1,0:T(8,128)S(1)}, f32[4,2,128,128]{3,2,1,0:T(8,128)S(1)}, s16[272,128]{1,0:T(8,128)(2,1)S(1)}, s16[272,128]{1,0:T(8,128)(2,1)S(1)}, s16[272,128]{1,0:T(8,128)(2,1)S(1)}) custom-call(s32[4]{0:T(128)S(1)} %pad_add_fusion.place_ref, bf16[256,2048]{1,0:T(8,128)(2,1)S(1)} %get-tuple-element.32.k_ref, ...), custom_call_target="tpu_custom_call" | custom-call | flops 134217728 | bytes 2883584 | tf_op jit(solution)/shard_map/chunk_states_1/pallas_call | solution.py:206
  31.2 0.7 collective-permute-start.7
  31.9 1.3 %collective-permute-start.8 = (s16[272,128]{1,0:T(8,128)(2,1)S(1)}, s16[272,128]{1,0:T(8,128)(2,1)S(1)}, u32[]{:S(2)}, u32[]{:S(2)}) collective-permute-start(s16[272,128]{1,0:T(8,128)(2,1)S(1)} %get-tuple-element.43), channel_id=1, source_target_pairs={{0,4},{2,6},{4,0},{6,2},{1,5},{3,7},{5,1},{7,3},{8,12},{10,14},{12... | collective-permute-start | bytes 208904 | tf_op jit(solution)/shard_map/ppermute | solution.py:437
  33.2 0.0 collective-permute-done.12.refs_5_.refs_6_
  33.2 1.6 %collective-permute-start.9 = (s16[272,128]{1,0:T(8,128)(2,1)S(1)}, s16[272,128]{1,0:T(8,128)(2,1)S(1)}, u32[]{:S(2)}, u32[]{:S(2)}) collective-permute-start(s16[272,128]{1,0:T(8,128)(2,1)S(1)} %get-tuple-element.44), channel_id=1, source_target_pairs={{0,6},{2,4},{4,2},{6,0},{1,7},{3,5},{5,3},{7,1},{8,14},{10,12},{12... | collective-permute-start | bytes 208904 | tf_op jit(solution)/shard_map/ppermute | solution.py:437
  34.8 0.0 collective-permute-done.11.refs_4_.refs_5_
  34.8 0.0 collective-permute-done.10.refs_3_.refs_4_
  34.8 0.8 carries_0.1
  35.5 1.4 %collective-permute-start.17 = (s16[272,128]{1,0:T(8,128)(2,1)S(1)}, s16[272,128]{1,0:T(8,128)(2,1)S(1)}, u32[]{:S(2)}, u32[]{:S(2)}) collective-permute-start(s16[272,128]{1,0:T(8,128)(2,1)S(1)} %get-tuple-element.47), channel_id=1, source_target_pairs={{0,6},{2,4},{4,2},{6,0},{1,7},{3,5},{5,3},{7,1},{8,14},{10,12},{12... | collective-permute-start | bytes 208904 | tf_op jit(solution)/shard_map/ppermute | solution.py:437
  36.9 0.7 collective-permute-start.16
  37.7 0.0 collective-permute-done.7.refs_0_.refs_8_
  37.7 0.7 collective-permute-done.9.refs_2_.refs_10_
  38.4 0.1 level_states_1.1.refs_2_
  38.5 2.3 %collective-permute-done.17.refs_1_ = s16[272,128]{1,0:T(8,128)(2,1)S(1)} collective-permute-done((s16[272,128]{1,0:T(8,128)(2,1)S(1)}, s16[272,128]{1,0:T(8,128)(2,1)S(1)}, u32[]{:S(2)}, u32[]{:S(2)}) %collective-permute-start.17) | collective-permute-done | bytes 69664 | tf_op jit(solution)/shard_map/ppermute | solution.py:437
  40.8 0.7 collective-permute-done.16.refs_0_
  41.5 1.9 %attend_0_1_3.1.refs_6_ = bf16[512,512]{1,0:T(8,128)(2,1)S(1)} custom-call(s32[4]{0:T(128)S(1)} %pad_add_fusion.place_ref, bf16[256,2048]{1,0:T(8,128)(2,1)S(1)} %get-tuple-element.30.refs_0_.q_ref, bf16[256,2048]{1,0:T(8,128)(2,1)S(1)} %collective-permute-done.refs_1_.q_sib_ref, bf16[256,2048]{1,0:T(8,128)(2,1)S(1)} %get-tuple-element.32.k_ref, ...), custom_call_target="tpu_custom_call" | custom-call | flops 402653184 | bytes 2097152 | tf_op jit(solution)/shard_map/attend_0_1_3/pallas_call | solution.py:362
  43.4 0.7 collective-permute-start.20
  44.1 1.3 %collective-permute-start.15 = (s16[272,128]{1,0:T(8,128)(2,1)S(1)}, s16[272,128]{1,0:T(8,128)(2,1)S(1)}, u32[]{:S(2)}, u32[]{:S(2)}) collective-permute-start(s16[272,128]{1,0:T(8,128)(2,1)S(1)} %level_states_1.1.refs_2_), channel_id=1, source_target_pairs={{0,8},{8,16},{16,24},{1,9},{9,17},{17,25},{2,10},{10,18},{18,26},{... | collective-permute-start | bytes 208904 | tf_op jit(solution)/shard_map/ppermute | solution.py:444
  45.4 4.2 %collective-permute-start.14 = (s16[272,128]{1,0:T(8,128)(2,1)S(1)}, s16[272,128]{1,0:T(8,128)(2,1)S(1)}, u32[]{:S(2)}, u32[]{:S(2)}) collective-permute-start(s16[272,128]{1,0:T(8,128)(2,1)S(1)} %level_states_1.1.refs_2_), channel_id=1, source_target_pairs={{0,16},{8,24},{1,17},{9,25},{2,18},{10,26},{3,19},{11,27},{4,20},{... | collective-permute-start | bytes 208904 | tf_op jit(solution)/shard_map/ppermute | solution.py:444
  49.6 1.3 %collective-permute-start.13 = (s16[272,128]{1,0:T(8,128)(2,1)S(1)}, s16[272,128]{1,0:T(8,128)(2,1)S(1)}, u32[]{:S(2)}, u32[]{:S(2)}) collective-permute-start(s16[272,128]{1,0:T(8,128)(2,1)S(1)} %level_states_1.1.refs_2_), channel_id=1, source_target_pairs={{0,24},{1,25},{2,26},{3,27},{4,28},{5,29},{6,30},{7,31}} | collective-permute-start | bytes 208904 | tf_op jit(solution)/shard_map/ppermute | solution.py:444
  51.0 0.6 collective-permute-done.14.refs_4_.refs_12_
  51.6 1.3 %collective-permute-done.13.refs_3_.refs_11_ = s16[272,128]{1,0:T(8,128)(2,1)S(1)} collective-permute-done((s16[272,128]{1,0:T(8,128)(2,1)S(1)}, s16[272,128]{1,0:T(8,128)(2,1)S(1)}, u32[]{:S(2)}, u32[]{:S(2)}) %collective-permute-start.13) | collective-permute-done | bytes 69664 | tf_op jit(solution)/shard_map/ppermute | solution.py:444
  52.9 0.7 carries_1.1
  53.6 1.5 %collective-permute-start.19 = (s16[272,128]{1,0:T(8,128)(2,1)S(1)}, s16[272,128]{1,0:T(8,128)(2,1)S(1)}, u32[]{:S(2)}, u32[]{:S(2)}) collective-permute-start(s16[272,128]{1,0:T(8,128)(2,1)S(1)} %get-tuple-element.49), channel_id=1, source_target_pairs={{0,2},{2,0},{4,6},{6,4},{1,3},{3,1},{5,7},{7,5},{8,10},{10,8},{12,... | collective-permute-start | bytes 208904 | tf_op jit(solution)/shard_map/ppermute | solution.py:437
  55.1 1.3 %collective-permute-start.18 = (s16[272,128]{1,0:T(8,128)(2,1)S(1)}, s16[272,128]{1,0:T(8,128)(2,1)S(1)}, u32[]{:S(2)}, u32[]{:S(2)}) collective-permute-start(s16[272,128]{1,0:T(8,128)(2,1)S(1)} %get-tuple-element.48), channel_id=1, source_target_pairs={{0,6},{2,4},{4,2},{6,0},{1,7},{3,5},{5,3},{7,1},{8,14},{10,12},{12... | collective-permute-start | bytes 208904 | tf_op jit(solution)/shard_map/ppermute | solution.py:437
  56.4 2.2 %collective-permute-done.19.refs_0_ = s16[272,128]{1,0:T(8,128)(2,1)S(1)} collective-permute-done((s16[272,128]{1,0:T(8,128)(2,1)S(1)}, s16[272,128]{1,0:T(8,128)(2,1)S(1)}, u32[]{:S(2)}, u32[]{:S(2)}) %collective-permute-start.19) | collective-permute-done | bytes 69664 | tf_op jit(solution)/shard_map/ppermute | solution.py:437
  58.6 1.3 %attend_1_1.1.refs_1_ = bf16[512,256]{1,0:T(8,128)(2,1)S(1)} custom-call(s32[4]{0:T(128)S(1)} %pad_add_fusion.place_ref, bf16[256,2048]{1,0:T(8,128)(2,1)S(1)} %get-tuple-element.30.refs_0_.q_ref, bf16[256,2048]{1,0:T(8,128)(2,1)S(1)} %collective-permute-done.refs_1_.q_sib_ref, bf16[256,2048]{1,0:T(8,128)(2,1)S(1)} %get-tuple-element.32.k_ref, ...), custom_call_target="tpu_custom_call" | custom-call | flops 201326592 | bytes 1048576 | tf_op jit(solution)/shard_map/attend_1_1/pallas_call | solution.py:362
  59.9 1.6 %collective-permute-start.23 = (bf16[512,256]{1,0:T(8,128)(2,1)S(1)}, bf16[512,256]{1,0:T(8,128)(2,1)S(1)}, u32[]{:S(2)}, u32[]{:S(2)}) collective-permute-start(bf16[512,256]{1,0:T(8,128)(2,1)S(1)} %attend_1_1.1.refs_1_), channel_id=1, source_target_pairs={{0,2},{2,0},{1,3},{3,1},{4,6},{6,4},{5,7},{7,5},{8,10},{10,8},{9,1... | collective-permute-start | bytes 786440 | tf_op jit(solution)/shard_map/ppermute | solution.py:437
  61.5 0.0 collective-permute-done.18.refs_0_
  61.6 0.0 collective-permute-done.20.refs_2_
  61.6 1.3 %attend_1_3.1.refs_14_.refs_2_ = bf16[512,256]{1,0:T(8,128)(2,1)S(1)} custom-call(s32[4]{0:T(128)S(1)} %pad_add_fusion.place_ref, bf16[256,2048]{1,0:T(8,128)(2,1)S(1)} %get-tuple-element.30.refs_0_.q_ref, bf16[256,2048]{1,0:T(8,128)(2,1)S(1)} %collective-permute-done.refs_1_.q_sib_ref, bf16[256,2048]{1,0:T(8,128)(2,1)S(1)} %get-tuple-element.32.k_ref, ...), custom_call_target="tpu_custom_call" | custom-call | flops 201326592 | bytes 1048576 | tf_op jit(solution)/shard_map/attend_1_3/pallas_call | solution.py:362
  62.9 1.1 %own_carries.1 = (s16[528,128]{1,0:T(8,128)(2,1)S(1)}, s16[528,128]{1,0:T(8,128)(2,1)S(1)}, f32[2,2,128,128]{3,2,1,0:T(8,128)S(1)}, f32[2,2,128,128]{3,2,1,0:T(8,128)S(1)}) custom-call(s32[4]{0:T(128)S(1)} %pad_add_fusion.place_ref, f32[2,128,128]{2,1,0:T(8,128)S(1)} %get-tuple-element.36.own_ref.refs_0_, ...), custom_call_target="tpu_custom_call" | custom-call | bytes 2490368 | tf_op jit(solution)/shard_map/own_carries/pallas_call | solution.py:304
  64.0 0.4 collective-permute-start.24
  64.5 0.9 %collective-permute-start.21 = (bf16[512,256]{1,0:T(8,128)(2,1)S(1)}, bf16[512,256]{1,0:T(8,128)(2,1)S(1)}, u32[]{:S(2)}, u32[]{:S(2)}) collective-permute-start(bf16[512,256]{1,0:T(8,128)(2,1)S(1)} %attend_1_3.1.refs_14_.refs_2_), channel_id=1, source_target_pairs={{0,2},{2,0},{1,3},{3,1},{4,6},{6,4},{5,7},{7,5},{8,10},{10,8},{9,1... | collective-permute-start | bytes 786440 | tf_op jit(solution)/shard_map/ppermute | solution.py:437
  65.4 1.2 %collective-permute-start.22 = (s16[528,128]{1,0:T(8,128)(2,1)S(1)}, s16[528,128]{1,0:T(8,128)(2,1)S(1)}, u32[]{:S(2)}, u32[]{:S(2)}) collective-permute-start(s16[528,128]{1,0:T(8,128)(2,1)S(1)} %get-tuple-element.51), channel_id=1, source_target_pairs={{0,4},{2,6},{4,0},{6,2},{1,5},{3,7},{5,1},{7,3},{8,12},{10,14},{12... | collective-permute-start | bytes 405512 | tf_op jit(solution)/shard_map/ppermute | solution.py:437
  66.6 5.3 %collective-permute-done.22.refs_1_ = s16[528,128]{1,0:T(8,128)(2,1)S(1)} collective-permute-done((s16[528,128]{1,0:T(8,128)(2,1)S(1)}, s16[528,128]{1,0:T(8,128)(2,1)S(1)}, u32[]{:S(2)}, u32[]{:S(2)}) %collective-permute-start.22) | collective-permute-done | bytes 135200 | tf_op jit(solution)/shard_map/ppermute | solution.py:437
  71.9 1.9 %attend_0_0_2.1.refs_2_.refs_0_ = bf16[512,512]{1,0:T(8,128)(2,1)S(1)} custom-call(s32[4]{0:T(128)S(1)} %pad_add_fusion.place_ref, bf16[256,2048]{1,0:T(8,128)(2,1)S(1)} %get-tuple-element.30.refs_0_.q_ref, bf16[256,2048]{1,0:T(8,128)(2,1)S(1)} %collective-permute-done.refs_1_.q_sib_ref, bf16[256,2048]{1,0:T(8,128)(2,1)S(1)} %get-tuple-element.32.k_ref, ...), custom_call_target="tpu_custom_call" | custom-call | flops 402653184 | bytes 2097152 | tf_op jit(solution)/shard_map/attend_0_0_2/pallas_call | solution.py:362
  73.8 1.9 %attend_1_0_2.1.refs_1_ = bf16[512,512]{1,0:T(8,128)(2,1)S(1)} custom-call(s32[4]{0:T(128)S(1)} %pad_add_fusion.place_ref, bf16[256,2048]{1,0:T(8,128)(2,1)S(1)} %get-tuple-element.30.refs_0_.q_ref, bf16[256,2048]{1,0:T(8,128)(2,1)S(1)} %collective-permute-done.refs_1_.q_sib_ref, bf16[256,2048]{1,0:T(8,128)(2,1)S(1)} %get-tuple-element.32.k_ref, ...), custom_call_target="tpu_custom_call" | custom-call | flops 402653184 | bytes 2097152 | tf_op jit(solution)/shard_map/attend_1_0_2/pallas_call | solution.py:362
  75.7 1.8 %assemble.1.refs_1_ = bf16[1024,1024]{1,0:T(8,128)(2,1)} custom-call(s32[4]{0:T(128)S(1)} %pad_add_fusion.place_ref, bf16[512,512]{1,0:T(8,128)(2,1)S(1)} %attend_0_0_2.1.refs_2_.refs_0_, bf16[512,512]{1,0:T(8,128)(2,1)S(1)} %attend_1_0_2.1.refs_1_, bf16[512,512]{1,0:T(8,128)(2,1)S(1)} %collective-permute-done.20.refs_2_, ...), custom_call_target="tpu_custom_call" | custom-call | tf_op jit(solution)/shard_map/assemble/pallas_call | solution.py:401
  77.5 0.0 collective-permute-done.24.refs_1_
  77.5 1.4 %assemble_cache.1 = f32[1,8,128,128]{3,2,1,0:T(8,128)} custom-call(s32[4]{0:T(128)S(1)} %pad_add_fusion.place_ref, f32[2,2,128,128]{3,2,1,0:T(8,128)S(1)} %get-tuple-element.52.refs_0_, f32[2,2,128,128]{3,2,1,0:T(8,128)S(1)} %collective-permute-done.24.refs_1_), custom_call_target="tpu_custom_call" | custom-call | tf_op jit(solution)/shard_map/assemble_cache/pallas_call | solution.py:422
  78.9 1.3 %finish.1 = bf16[1024,1024]{1,0:T(8,128)(2,1)} custom-call(s32[4]{0:T(128)S(1)} %pad_add_fusion.place_ref, bf16[512,256]{1,0:T(8,128)(2,1)S(1)} %collective-permute-done.21.refs_0_, bf16[1024,1024]{1,0:T(8,128)(2,1)} %assemble.1.refs_1_), custom_call_target="tpu_custom_call", output_to_operand_aliasing={{}: (2, {})} | custom-call | tf_op jit(solution)/shard_map/finish/pallas_call | solution.py:401
  (8 shorter events, 0.0 us)
Async XLA Ops:
  0.7 5.0 %copy-start = (bf16[256,4096]{1,0:T(8,128)(2,1)S(1)}, bf16[256,4096]{1,0:T(8,128)(2,1)}, u32[]{:S(2)}) copy-start(bf16[256,4096]{1,0:T(8,128)(2,1)} %queries_ref.1) | copy-start | bytes 6291460
  5.1 2.8 %collective-permute-start.1 = (bf16[256,2048]{1,0:T(8,128)(2,1)S(1)}, bf16[256,2048]{1,0:T(8,128)(2,1)S(1)}, u32[]{:S(2)}, u32[]{:S(2)}) collective-permute-start(bf16[256,2048]{1,0:T(8,128)(2,1)S(1)} %get-tuple-element.33), channel_id=1, source_target_pairs={{0,1},{1,0},{2,3},{3,2},{4,5},{5,4},{6,7},{7,6},{8,9},{9,8},{10,11... | collective-permute-start | bytes 3145736 | tf_op jit(solution)/shard_map/ppermute | solution.py:437
  5.6 3.8 %collective-permute-start.2 = (bf16[256,2048]{1,0:T(8,128)(2,1)S(1)}, bf16[256,2048]{1,0:T(8,128)(2,1)S(1)}, u32[]{:S(2)}, u32[]{:S(2)}) collective-permute-start(bf16[256,2048]{1,0:T(8,128)(2,1)S(1)} %get-tuple-element.35), channel_id=1, source_target_pairs={{0,1},{1,0},{2,3},{3,2},{4,5},{5,4},{6,7},{7,6},{8,9},{9,8},{10,11... | collective-permute-start | bytes 3145736 | tf_op jit(solution)/shard_map/ppermute | solution.py:437
  6.4 23.4 %collective-permute-start = (bf16[256,2048]{1,0:T(8,128)(2,1)S(1)}, bf16[256,2048]{1,0:T(8,128)(2,1)S(1)}, u32[]{:S(2)}, u32[]{:S(2)}) collective-permute-start(bf16[256,2048]{1,0:T(8,128)(2,1)S(1)} %get-tuple-element.31), channel_id=1, source_target_pairs={{0,1},{1,0},{2,3},{3,2},{4,5},{5,4},{6,7},{7,6},{8,9},{9,8},{10,11... | collective-permute-start | bytes 3145736 | tf_op jit(solution)/shard_map/ppermute | solution.py:437
  9.4 5.9 %copy-start.1 = (f32[1024]{0:T(1024)S(1)}, f32[1024]{0:T(1024)}, u32[]{:S(2)}) copy-start(f32[1024]{0:T(1024)} %param.9) | copy-start | bytes 12292
  10.8 8.3 %collective-permute-start.3 = (s16[272,128]{1,0:T(8,128)(2,1)S(1)}, s16[272,128]{1,0:T(8,128)(2,1)S(1)}, u32[]{:S(2)}, u32[]{:S(2)}) collective-permute-start(s16[272,128]{1,0:T(8,128)(2,1)S(1)} %get-tuple-element.37), channel_id=1, source_target_pairs={{0,2},{2,0},{4,6},{6,4},{1,3},{3,1},{5,7},{7,5},{8,10},{10,8},{12,... | collective-permute-start | bytes 208904 | tf_op jit(solution)/shard_map/ppermute | solution.py:437
  13.7 5.4 %collective-permute-start.4 = (s16[272,128]{1,0:T(8,128)(2,1)S(1)}, s16[272,128]{1,0:T(8,128)(2,1)S(1)}, u32[]{:S(2)}, u32[]{:S(2)}) collective-permute-start(s16[272,128]{1,0:T(8,128)(2,1)S(1)} %get-tuple-element.38), channel_id=1, source_target_pairs={{0,4},{2,6},{4,0},{6,2},{1,5},{3,7},{5,1},{7,3},{8,12},{10,14},{12... | collective-permute-start | bytes 208904 | tf_op jit(solution)/shard_map/ppermute | solution.py:437
  15.2 5.2 %collective-permute-start.5 = (s16[272,128]{1,0:T(8,128)(2,1)S(1)}, s16[272,128]{1,0:T(8,128)(2,1)S(1)}, u32[]{:S(2)}, u32[]{:S(2)}) collective-permute-start(s16[272,128]{1,0:T(8,128)(2,1)S(1)} %get-tuple-element.39), channel_id=1, source_target_pairs={{0,6},{2,4},{4,2},{6,0},{1,7},{3,5},{5,3},{7,1},{8,14},{10,12},{12... | collective-permute-start | bytes 208904 | tf_op jit(solution)/shard_map/ppermute | solution.py:437
  15.3 3.8 %collective-permute-start.6 = (f32[1,1024]{1,0:T(1,128)S(1)}, f32[1,1024]{1,0:T(1,128)S(1)}, u32[]{:S(2)}, u32[]{:S(2)}) collective-permute-start(f32[1,1024]{1,0:T(1,128)S(1)} %bitcast.5), channel_id=1, source_target_pairs={{0,2},{2,0},{1,3},{3,1},{4,6},{6,4},{5,7},{7,5},{8,10},{10,8},{9,1... | collective-permute-start | bytes 12296 | tf_op jit(solution)/shard_map/ppermute | solution.py:437
  20.5 12.7 %collective-permute-start.12 = (s16[272,128]{1,0:T(8,128)(2,1)S(1)}, s16[272,128]{1,0:T(8,128)(2,1)S(1)}, u32[]{:S(2)}, u32[]{:S(2)}) collective-permute-start(s16[272,128]{1,0:T(8,128)(2,1)S(1)} %level_states_0.1.refs_0_), channel_id=1, source_target_pairs={{0,8},{8,16},{16,24},{1,9},{9,17},{17,25},{2,10},{10,18},{18,26},{... | collective-permute-start | bytes 208904 | tf_op jit(solution)/shard_map/ppermute | solution.py:444
  24.0 10.7 %collective-permute-start.11 = (s16[272,128]{1,0:T(8,128)(2,1)S(1)}, s16[272,128]{1,0:T(8,128)(2,1)S(1)}, u32[]{:S(2)}, u32[]{:S(2)}) collective-permute-start(s16[272,128]{1,0:T(8,128)(2,1)S(1)} %level_states_0.1.refs_0_), channel_id=1, source_target_pairs={{0,16},{8,24},{1,17},{9,25},{2,18},{10,26},{3,19},{11,27},{4,20},{... | collective-permute-start | bytes 208904 | tf_op jit(solution)/shard_map/ppermute | solution.py:444
  28.5 6.2 %collective-permute-start.10 = (s16[272,128]{1,0:T(8,128)(2,1)S(1)}, s16[272,128]{1,0:T(8,128)(2,1)S(1)}, u32[]{:S(2)}, u32[]{:S(2)}) collective-permute-start(s16[272,128]{1,0:T(8,128)(2,1)S(1)} %level_states_0.1.refs_0_), channel_id=1, source_target_pairs={{0,24},{1,25},{2,26},{3,27},{4,28},{5,29},{6,30},{7,31}} | collective-permute-start | bytes 208904 | tf_op jit(solution)/shard_map/ppermute | solution.py:444
  31.2 6.4 %collective-permute-start.7 = (s16[272,128]{1,0:T(8,128)(2,1)S(1)}, s16[272,128]{1,0:T(8,128)(2,1)S(1)}, u32[]{:S(2)}, u32[]{:S(2)}) collective-permute-start(s16[272,128]{1,0:T(8,128)(2,1)S(1)} %get-tuple-element.42), channel_id=1, source_target_pairs={{0,2},{2,0},{4,6},{6,4},{1,3},{3,1},{5,7},{7,5},{8,10},{10,8},{12,... | collective-permute-start | bytes 208904 | tf_op jit(solution)/shard_map/ppermute | solution.py:437
  31.9 5.8 %collective-permute-start.8 = (s16[272,128]{1,0:T(8,128)(2,1)S(1)}, s16[272,128]{1,0:T(8,128)(2,1)S(1)}, u32[]{:S(2)}, u32[]{:S(2)}) collective-permute-start(s16[272,128]{1,0:T(8,128)(2,1)S(1)} %get-tuple-element.43), channel_id=1, source_target_pairs={{0,4},{2,6},{4,0},{6,2},{1,5},{3,7},{5,1},{7,3},{8,12},{10,14},{12... | collective-permute-start | bytes 208904 | tf_op jit(solution)/shard_map/ppermute | solution.py:437
  33.2 5.2 %collective-permute-start.9 = (s16[272,128]{1,0:T(8,128)(2,1)S(1)}, s16[272,128]{1,0:T(8,128)(2,1)S(1)}, u32[]{:S(2)}, u32[]{:S(2)}) collective-permute-start(s16[272,128]{1,0:T(8,128)(2,1)S(1)} %get-tuple-element.44), channel_id=1, source_target_pairs={{0,6},{2,4},{4,2},{6,0},{1,7},{3,5},{5,3},{7,1},{8,14},{10,12},{12... | collective-permute-start | bytes 208904 | tf_op jit(solution)/shard_map/ppermute | solution.py:437
  35.5 5.3 %collective-permute-start.17 = (s16[272,128]{1,0:T(8,128)(2,1)S(1)}, s16[272,128]{1,0:T(8,128)(2,1)S(1)}, u32[]{:S(2)}, u32[]{:S(2)}) collective-permute-start(s16[272,128]{1,0:T(8,128)(2,1)S(1)} %get-tuple-element.47), channel_id=1, source_target_pairs={{0,6},{2,4},{4,2},{6,0},{1,7},{3,5},{5,3},{7,1},{8,14},{10,12},{12... | collective-permute-start | bytes 208904 | tf_op jit(solution)/shard_map/ppermute | solution.py:437
  36.9 4.6 %collective-permute-start.16 = (s16[272,128]{1,0:T(8,128)(2,1)S(1)}, s16[272,128]{1,0:T(8,128)(2,1)S(1)}, u32[]{:S(2)}, u32[]{:S(2)}) collective-permute-start(s16[272,128]{1,0:T(8,128)(2,1)S(1)} %get-tuple-element.45.refs_3_), channel_id=1, source_target_pairs={{0,2},{2,0},{4,6},{6,4},{1,3},{3,1},{5,7},{7,5},{8,10},{10,8},{12,... | collective-permute-start | bytes 208904 | tf_op jit(solution)/shard_map/ppermute | solution.py:437
  43.4 18.1 %collective-permute-start.20 = (bf16[512,512]{1,0:T(8,128)(2,1)S(1)}, bf16[512,512]{1,0:T(8,128)(2,1)S(1)}, u32[]{:S(2)}, u32[]{:S(2)}) collective-permute-start(bf16[512,512]{1,0:T(8,128)(2,1)S(1)} %attend_0_1_3.1.refs_6_), channel_id=1, source_target_pairs={{0,2},{2,0},{1,3},{3,1},{4,6},{6,4},{5,7},{7,5},{8,10},{10,8},{9,1... | collective-permute-start | bytes 1572872 | tf_op jit(solution)/shard_map/ppermute | solution.py:437
  44.1 6.8 %collective-permute-start.15 = (s16[272,128]{1,0:T(8,128)(2,1)S(1)}, s16[272,128]{1,0:T(8,128)(2,1)S(1)}, u32[]{:S(2)}, u32[]{:S(2)}) collective-permute-start(s16[272,128]{1,0:T(8,128)(2,1)S(1)} %level_states_1.1.refs_2_), channel_id=1, source_target_pairs={{0,8},{8,16},{16,24},{1,9},{9,17},{17,25},{2,10},{10,18},{18,26},{... | collective-permute-start | bytes 208904 | tf_op jit(solution)/shard_map/ppermute | solution.py:444
  45.4 6.2 %collective-permute-start.14 = (s16[272,128]{1,0:T(8,128)(2,1)S(1)}, s16[272,128]{1,0:T(8,128)(2,1)S(1)}, u32[]{:S(2)}, u32[]{:S(2)}) collective-permute-start(s16[272,128]{1,0:T(8,128)(2,1)S(1)} %level_states_1.1.refs_2_), channel_id=1, source_target_pairs={{0,16},{8,24},{1,17},{9,25},{2,18},{10,26},{3,19},{11,27},{4,20},{... | collective-permute-start | bytes 208904 | tf_op jit(solution)/shard_map/ppermute | solution.py:444
  49.6 3.2 %collective-permute-start.13 = (s16[272,128]{1,0:T(8,128)(2,1)S(1)}, s16[272,128]{1,0:T(8,128)(2,1)S(1)}, u32[]{:S(2)}, u32[]{:S(2)}) collective-permute-start(s16[272,128]{1,0:T(8,128)(2,1)S(1)} %level_states_1.1.refs_2_), channel_id=1, source_target_pairs={{0,24},{1,25},{2,26},{3,27},{4,28},{5,29},{6,30},{7,31}} | collective-permute-start | bytes 208904 | tf_op jit(solution)/shard_map/ppermute | solution.py:444
  53.6 5.0 %collective-permute-start.19 = (s16[272,128]{1,0:T(8,128)(2,1)S(1)}, s16[272,128]{1,0:T(8,128)(2,1)S(1)}, u32[]{:S(2)}, u32[]{:S(2)}) collective-permute-start(s16[272,128]{1,0:T(8,128)(2,1)S(1)} %get-tuple-element.49), channel_id=1, source_target_pairs={{0,2},{2,0},{4,6},{6,4},{1,3},{3,1},{5,7},{7,5},{8,10},{10,8},{12,... | collective-permute-start | bytes 208904 | tf_op jit(solution)/shard_map/ppermute | solution.py:437
  55.1 6.5 %collective-permute-start.18 = (s16[272,128]{1,0:T(8,128)(2,1)S(1)}, s16[272,128]{1,0:T(8,128)(2,1)S(1)}, u32[]{:S(2)}, u32[]{:S(2)}) collective-permute-start(s16[272,128]{1,0:T(8,128)(2,1)S(1)} %get-tuple-element.48), channel_id=1, source_target_pairs={{0,6},{2,4},{4,2},{6,0},{1,7},{3,5},{5,3},{7,1},{8,14},{10,12},{12... | collective-permute-start | bytes 208904 | tf_op jit(solution)/shard_map/ppermute | solution.py:437
  59.9 15.8 %collective-permute-start.23 = (bf16[512,256]{1,0:T(8,128)(2,1)S(1)}, bf16[512,256]{1,0:T(8,128)(2,1)S(1)}, u32[]{:S(2)}, u32[]{:S(2)}) collective-permute-start(bf16[512,256]{1,0:T(8,128)(2,1)S(1)} %attend_1_1.1.refs_1_), channel_id=1, source_target_pairs={{0,2},{2,0},{1,3},{3,1},{4,6},{6,4},{5,7},{7,5},{8,10},{10,8},{9,1... | collective-permute-start | bytes 786440 | tf_op jit(solution)/shard_map/ppermute | solution.py:437
  64.0 13.5 %collective-permute-start.24 = (f32[2,2,128,128]{3,2,1,0:T(8,128)S(1)}, f32[2,2,128,128]{3,2,1,0:T(8,128)S(1)}, u32[]{:S(2)}, u32[]{:S(2)}) collective-permute-start(f32[2,2,128,128]{3,2,1,0:T(8,128)S(1)} %get-tuple-element.53), channel_id=1, source_target_pairs={{0,4},{4,0},{1,5},{5,1},{2,6},{6,2},{3,7},{7,3},{8,12},{12,8},{9,1... | collective-permute-start | bytes 786440 | tf_op jit(solution)/shard_map/ppermute | solution.py:437
  64.5 14.4 %collective-permute-start.21 = (bf16[512,256]{1,0:T(8,128)(2,1)S(1)}, bf16[512,256]{1,0:T(8,128)(2,1)S(1)}, u32[]{:S(2)}, u32[]{:S(2)}) collective-permute-start(bf16[512,256]{1,0:T(8,128)(2,1)S(1)} %attend_1_3.1.refs_14_.refs_2_), channel_id=1, source_target_pairs={{0,2},{2,0},{1,3},{3,1},{4,6},{6,4},{5,7},{7,5},{8,10},{10,8},{9,1... | collective-permute-start | bytes 786440 | tf_op jit(solution)/shard_map/ppermute | solution.py:437
  65.4 6.5 %collective-permute-start.22 = (s16[528,128]{1,0:T(8,128)(2,1)S(1)}, s16[528,128]{1,0:T(8,128)(2,1)S(1)}, u32[]{:S(2)}, u32[]{:S(2)}) collective-permute-start(s16[528,128]{1,0:T(8,128)(2,1)S(1)} %get-tuple-element.51), channel_id=1, source_target_pairs={{0,4},{2,6},{4,0},{6,2},{1,5},{3,7},{5,1},{7,3},{8,12},{10,14},{12... | collective-permute-start | bytes 405512 | tf_op jit(solution)/shard_map/ppermute | solution.py:437

commit v6 on v5

--- a/solution.py
+++ b/solution.py
@@ -155,18 +155,29 @@
     ref[len(states) * HD :] = exponents.astype(jnp.int32).astype(jnp.int16)
 
 
-def decoded(ref):
+def decoded(ref, which=None):
     count = ref.shape[0] // HD
     exponents = ref[count * HD :].astype(jnp.int32).astype(jnp.float32)
     return [
         ref[i * HD : (i + 1) * HD].astype(jnp.int32).astype(jnp.float32)
         * jnp.exp2(exponents[i : i + 1] - 15)
-        for i in range(count)
+        for i in which or range(count)
     ]
 
 
 def plus(left, right):
     return [a + b for a, b in zip(left, right)]
+
+
+def states_in(ref, which):
+    return decoded(ref, which) if ref.dtype == jnp.int16 else [ref[i] for i in which]
+
+
+def total_of(refs, which):
+    total = [jnp.zeros((HD, HD), jnp.float32)] * len(which)
+    for ref in refs:
+        total = plus(total, states_in(ref, which))
+    return total
 
 
 def coded_shape(heads):
@@ -184,45 +195,48 @@
     return pl.ds(pl.multiple_of(start, HD), HD)
 
 
-def chunk_states(plan, place, key, value, half, after):
+def chunk_states(plan, place, key, value, after):
+    owned = plan.halves * plan.each
+
     def kernel(place_ref, k_ref, k_sib_ref, v_ref, v_sib_ref, *refs):
         own_ref, first_ref, *send_refs = refs[len(after) :]
         is_first = jnp.full((HD, HD), place_ref[0], jnp.int32) == 0
-        for offset in (*range(1, plan.plane), 0):
+        for offset in (*range(plan.plane - 1, 0, -1), 0):
             states = []
-            for i in range(plan.each):
-                at = owned_columns(plan, place_ref, offset, half, i)
+            for n in range(owned):
+                at = owned_columns(plan, place_ref, offset, *divmod(n, plan.each))
                 mine = contract_rows(v_ref[:, at], k_ref[:, at])
                 sib = contract_rows(v_sib_ref[:, at], k_sib_ref[:, at])
-                first_ref[offset, i] = jnp.where(is_first, mine, sib)
+                first_ref[offset, n] = jnp.where(is_first, mine, sib)
                 states.append(mine + sib)
             if offset:
                 code(states, send_refs[offset - 1])
             else:
-                for i, state in enumerate(states):
-                    own_ref[i] = state
-
-    heads = plan.plane * plan.each
-    return pl.pallas_call(
-        kernel,
-        out_shape=[states_shape(plan.each), states_shape(plan.plane, plan.each)]
-        + [coded_shape(plan.each)] * (plan.plane - 1),
+                for n, state in enumerate(states):
+                    own_ref[n] = state
+
+    heads = plan.plane * owned
+    return pl.pallas_call(
+        kernel,
+        out_shape=[states_shape(owned), states_shape(plan.plane, owned)]
+        + [coded_shape(owned)] * (plan.plane - 1),
         in_specs=[SMEM] + [VMEM] * 4 + [ANY] * len(after),
         out_specs=[VMEM] * (1 + plan.plane),
         compiler_params=params(),
         cost_estimate=cost(
             4 * plan.rows * HD * HD * heads, 8 * plan.rows * HD * heads + 6 * heads * HD * HD
         ),
-        name=f"chunk_states_{half}",
+        name="chunk_states",
     )(place, *key, *value, *after)
+
+
+def of_half(plan, half):
+    return range(half * plan.each, (half + 1) * plan.each)
 
 
 def level_states(plan, own, others, half, after):
     def kernel(own_ref, *refs):
-        total = [own_ref[i] for i in range(plan.each)]
-        for ref in refs[: len(others)]:
-            total = plus(total, decoded(ref))
-        code(total, refs[-1])
+        code(total_of((own_ref, *refs[: len(others)]), of_half(plan, half)), refs[-1])
 
     return pl.pallas_call(
         kernel,
@@ -235,13 +249,27 @@
     )(own, *others, *after)
 
 
-def carried(plan, place_ref, own, others, levels, offsets):
+def earlier_levels(plan, levels, after):
+    def kernel(*refs):
+        for i, state in enumerate(total_of(refs[: len(levels)], range(plan.each))):
+            refs[-1][i] = state
+
+    return pl.pallas_call(
+        kernel,
+        out_shape=states_shape(plan.each),
+        in_specs=[VMEM] * len(levels) + [ANY] * len(after),
+        out_specs=VMEM,
+        compiler_params=params(),
+        cost_estimate=cost(0, len(levels) * plan.each * HD * HD * 2),
+        name="earlier_levels",
+    )(*levels, *after)
+
+
+def carried(plan, place_ref, own, others, levels, half, offsets):
     x, y = place_ref[1], place_ref[2]
     here = x * plan.n_y + y
-    earlier = [jnp.zeros((HD, HD), jnp.float32)] * plan.each
-    for ref in levels:
-        earlier = plus(earlier, decoded(ref))
-    states = [[own[i] for i in range(plan.each)]] + [decoded(ref) for ref in others]
+    earlier = total_of(levels, range(plan.each))
+    states = [states_in(ref, of_half(plan, half)) for ref in (own, *others)]
 
     def add(totals, keep_of):
         for offset, terms in enumerate(states):
@@ -261,9 +289,8 @@
     n_others, n_levels = len(others), len(levels)
 
     def kernel(place_ref, own_ref, *refs):
-        before, _ = carried(
-            plan, place_ref, own_ref, refs[:n_others], refs[n_others : n_others + n_levels], offsets
-        )
+        others_refs, level_refs = refs[:n_others], refs[n_others : n_others + n_levels]
+        before, _ = carried(plan, place_ref, own_ref, others_refs, level_refs, half, offsets)
         for states, ref in zip(before, refs[n_others + n_levels + len(after) :]):
             code(states, ref)
 
@@ -279,16 +306,17 @@
 
 
 def own_carries(plan, place, own, others, levels, offsets, after):
-    n_others, n_levels = len(others[0]), len(levels[0])
-    each_half = 1 + n_others + n_levels
-
-    def kernel(place_ref, *refs):
-        outs = refs[plan.halves * each_half + len(after) :]
+    n_others = len(others)
+    starts = [1 + n_others + sum(map(len, levels[:h])) for h in range(plan.halves + 1)]
+
+    def kernel(place_ref, own_ref, *refs):
+        refs = (own_ref, *refs)
+        outs = refs[starts[-1] + len(after) :]
         befores = [[] for _ in offsets]
         for half in range(plan.halves):
-            own_ref, *of_half = refs[half * each_half : (half + 1) * each_half]
+            level_refs = refs[starts[half] : starts[half + 1]]
             before, blocks = carried(
-                plan, place_ref, own_ref, of_half[:n_others], of_half[n_others:], offsets
+                plan, place_ref, own_ref, refs[1 : starts[0]], level_refs, half, offsets
             )
             for all_states, states in zip(befores, before):
                 all_states.extend(states)
@@ -300,17 +328,16 @@
         for states, ref in zip(befores, outs):
             code(states, ref)
 
-    operands = [a for h in range(plan.halves) for a in (own[h], *others[h], *levels[h])]
     return pl.pallas_call(
         kernel,
         out_shape=[coded_shape(plan.halves * plan.each)] * len(offsets)
         + [states_shape(plan.halves, plan.each)] * plan.n_inner,
-        in_specs=[SMEM] + [VMEM] * len(operands) + [ANY] * len(after),
+        in_specs=[SMEM] + [VMEM] * starts[-1] + [ANY] * len(after),
         out_specs=[VMEM] * (len(offsets) + plan.n_inner),
         compiler_params=params(),
-        cost_estimate=cost(0, (plan.plane * 4 + n_levels) * plan.each * HD * HD * 4),
+        cost_estimate=cost(0, plan.plane * plan.each * HD * HD * 20),
         name="own_carries",
-    )(place, *operands, *after)
+    )(place, own, *others, *[a for arrays in levels for a in arrays], *after)
 
 
 def attend(plan, place, query, key, value, carry, first, gain, half, offsets, after=()):
@@ -348,7 +375,7 @@
                 start = ((half * plan.n_inner + x) * plan.each + i) * HD
                 gain = gain_ref[:, pl.ds(pl.multiple_of(start, HD), HD)]
                 out_at = slice(piece * plan.piece + i * HD, piece * plan.piece + (i + 1) * HD)
-                first = first_ref[offset, i]
+                first = first_ref[offset, half * plan.each + i]
                 mine = carry_states[skip + i] + jnp.where(is_second, first, 0.0)
                 sib = carry_states[skip + i] + jnp.where(is_second, 0.0, first)
                 out_ref[pl.ds(pl.multiple_of(core * rows, rows), rows), out_at] = attended(
@@ -450,18 +477,14 @@
     query, query_out = spike_queries(plan, place, queries, counts)
     query = (query, swap(query_out, "core", 1, CORES))
 
-    own, first, others, levels, coded = [], [], [], [], []
-
-    def owner_stage(half, after):
-        mine, parts, *sends = chunk_states(plan, place, key, value, half, after)
-        own.append(mine)
-        first.append(parts)
-        others.append([in_level(a, o) for o, a in enumerate(sends, 1)])
-
-    def level_stage(half, after):
-        level = level_states(plan, own[half], others[half], half, after)
-        coded.append(level)
+    own, first, *sends = chunk_states(plan, place, key, value, [query[0]])
+    others = [in_level(a, o) for o, a in enumerate(sends, 1)]
+    levels = []
+    after = [query[1], *gains[1:]]
+    for half in halves:
+        level = level_states(plan, own, others, half, after)
         levels.append([to_later(level, d) for d in range(plan.n_outer - 1, 0, -1)])
+        after = [level]
 
     of_group = [list(range(y, plan.plane, plan.n_y)) for y in range(plan.n_y)]
     abroad = [o for offsets in of_group[1:] for o in offsets]
@@ -474,7 +497,7 @@
             key,
             value,
             [carry[o] for o in offsets],
-            first[half],
+            first,
             gains[offsets[0] % plan.n_y],
             half,
             offsets,
@@ -482,7 +505,7 @@
         )
 
     def carry_stage(half, after):
-        sends = carries(plan, place, own[half], others[half], levels[half], half, abroad, after)
+        sends = carries(plan, place, own, others, levels[half], half, abroad, after)
         return sends[0], {o: in_level(a, o) for o, a in zip(abroad, sends)}
 
     parts = []
@@ -498,14 +521,12 @@
                 after = [part]
         return after
 
-    owner_stage(0, [query[0]])
-    level_stage(0, gains[1:])
-    if plan.halves > 1:
-        owner_stage(1, [coded[0], query[1]])
-    done, carry = carry_stage(0, [own[-1]])
-    if plan.halves > 1:
-        level_stage(1, [done])
-    after = send_stage(0, carry, [coded[-1]])
+    done, carry = carry_stage(0, after)
+    after = []
+    if plan.halves > 1 and levels[1]:
+        levels[1] = [earlier_levels(plan, levels[1], [done])]
+        after = levels[1]
+    after = send_stage(0, carry, after)
     if plan.halves > 1:
         _, carry = carry_stage(1, after)
         after = send_stage(1, carry, [])

time: 80.4 us -> 80.7 us (level)
  waiting for transfers between devices: 18.9 us -> 25.3 us
  starting transfers between devices: 37 us -> 31.4 us
    ppermute x19 -> x16, waiting for transfers between devices: 17 us -> 25.3 us  [swap(): return lax.ppermute(array, axes, [(i, i ^ offset) for i in range(size)])]
    ppermute x6, starting transfers between devices: 16.1 us -> 13.3 us  [to_later(): return lax.ppermute(array, 'outer', pairs)]
    ppermute x19 -> x16, starting transfers between devices: 20.9 us -> 18.1 us  [swap(): return lax.ppermute(array, axes, [(i, i ^ offset) for i in range(size)])]
    ppermute x6, waiting for transfers between devices: 1.92 us -> 0.02 us  [to_later(): return lax.ppermute(array, 'outer', pairs)]
  transfers between devices with their start and end apart: 25 -> 22, of which waited for: 11 -> 9; matrix products, arithmetic and copies ran while one was open for 0% -> 0% of each run, Pallas kernels for 20% -> 19%
where the time goes in v6:
time: 80.7 us; the launch traced here: 80.4 us
  starting transfers between devices  31.4 us (39%)
  waiting for transfers between devices  25.3 us (31%)
  Pallas kernels  22.8 us (28%)
  between operations  0.83 us (1%)
    ppermute x16, waiting for transfers between devices, swap(): return lax.ppermute(array, axes, [(i, i ^ offset) for i in range(size)])  25.3 us
    ppermute x16, starting transfers between devices, swap(): return lax.ppermute(array, axes, [(i, i ^ offset) for i in range(size)])  18.1 us
    ppermute x6, starting transfers between devices, to_later(): return lax.ppermute(array, 'outer', pairs)  13.3 us
    pallas_call x5, Pallas kernels, attend(): pl.pallas_call(kernel, out_shape=jax.ShapeDtypeStruct((CORES * rows, head...  8.29 us
    pallas_call x1, Pallas kernels, decode(): pl.pallas_call(kernel, out_shape=[jax.ShapeDtypeStruct((rows, plan.n_y *...  4.36 us
    pallas_call x2, Pallas kernels, assemble(): pl.pallas_call(kernel, out_shape=jax.ShapeDtypeStruct((plan.n_y * rows, p...  3.08 us
    pallas_call x1, Pallas kernels, chunk_states(): pl.pallas_call(kernel, out_shape=[states_shape(owned), states_shape(plan....  2.12 us
  transfers between devices with their start and end apart: 22, of which 9 were waited for; matrix products, arithmetic and copies ran while one was open for 0% of the time, Pallas kernels for 19%

profile of v6, /device:TPU:0, one launch (start us, length us, event | category | flops | bytes accessed | tf_op | source)
XLA Modules:
  0.0 80.4 jit_solution(12706788664542957674)
XLA Ops:
  0.6 0.1 pad_add_fusion.place_ref
  0.7 4.4 %decode.1 = (bf16[256,2048]{1,0:T(8,128)(2,1)S(1)}, bf16[256,2048]{1,0:T(8,128)(2,1)S(1)}, bf16[256,2048]{1,0:T(8,128)(2,1)S(1)}, bf16[256,2048]{1,0:T(8,128)(2,...) custom-call(s32[4]{0:T(128)S(1)} %pad_add_fusion.place_ref, s32[256,4096]{1,0:T(8,128)} %refs_0_.1, ...), custom_call_target="tpu_custom_call" | custom-call | flops 4194304 | bytes 14680064 | tf_op jit(solution)/shard_map/decode/pallas_call | solution.py:100
  5.1 0.5 collective-permute-start.1
  5.6 0.1 collective-permute-start.2
  5.7 0.0 copy-done
  5.7 0.8 spike_queries.1
  6.4 0.5 collective-permute-start
  6.9 0.9 %collective-permute-done.1.k_sib_ref = bf16[256,2048]{1,0:T(8,128)(2,1)S(1)} collective-permute-done((bf16[256,2048]{1,0:T(8,128)(2,1)S(1)}, bf16[256,2048]{1,0:T(8,128)(2,1)S(1)}, u32[]{:S(2)}, u32[]{:S(2)}) %collective-permute-start.1) | collective-permute-done | bytes 1048608 | tf_op jit(solution)/shard_map/ppermute | solution.py:464
  7.9 1.5 %collective-permute-done.2.v_sib_ref = bf16[256,2048]{1,0:T(8,128)(2,1)S(1)} collective-permute-done((bf16[256,2048]{1,0:T(8,128)(2,1)S(1)}, bf16[256,2048]{1,0:T(8,128)(2,1)S(1)}, u32[]{:S(2)}, u32[]{:S(2)}) %collective-permute-start.2) | collective-permute-done | bytes 1048608 | tf_op jit(solution)/shard_map/ppermute | solution.py:464
  9.4 2.1 %chunk_states.1 = (f32[4,128,128]{2,1,0:T(8,128)S(1)}, f32[4,4,128,128]{3,2,1,0:T(8,128)S(1)}, s16[528,128]{1,0:T(8,128)(2,1)S(1)}, s16[528,128]{1,0:T(8,128)(2,1)S(1)}, s16[528,128]{1,0:T(8,128)(2,1)S(1)}) custom-call(s32[4]{0:T(128)S(1)} %pad_add_fusion.place_ref, bf16[256,2048]{1,0:T(8,128)(2,1)S(1)} %get-tuple-element.27.k_ref, ...), custom_call_target="tpu_custom_call" | custom-call | flops 268435456 | bytes 5767168 | tf_op jit(solution)/shard_map/chunk_states/pallas_call | solution.py:219
  11.5 3.0 %collective-permute-start.4 = (s16[528,128]{1,0:T(8,128)(2,1)S(1)}, s16[528,128]{1,0:T(8,128)(2,1)S(1)}, u32[]{:S(2)}, u32[]{:S(2)}) collective-permute-start(s16[528,128]{1,0:T(8,128)(2,1)S(1)} %get-tuple-element.33), channel_id=1, source_target_pairs={{0,2},{2,0},{4,6},{6,4},{1,3},{3,1},{5,7},{7,5},{8,10},{10,8},{12,... | collective-permute-start | bytes 405512 | tf_op jit(solution)/shard_map/ppermute | solution.py:464
  14.5 1.5 %collective-permute-start.5 = (s16[528,128]{1,0:T(8,128)(2,1)S(1)}, s16[528,128]{1,0:T(8,128)(2,1)S(1)}, u32[]{:S(2)}, u32[]{:S(2)}) collective-permute-start(s16[528,128]{1,0:T(8,128)(2,1)S(1)} %get-tuple-element.34), channel_id=1, source_target_pairs={{0,4},{2,6},{4,0},{6,2},{1,5},{3,7},{5,1},{7,3},{8,12},{10,14},{12... | collective-permute-start | bytes 405512 | tf_op jit(solution)/shard_map/ppermute | solution.py:464
  16.0 0.1 collective-permute-start.6
  16.0 0.0 copy-done.1
  16.0 1.9 %collective-permute-start.3 = (f32[1,1024]{1,0:T(1,128)S(1)}, f32[1,1024]{1,0:T(1,128)S(1)}, u32[]{:S(2)}, u32[]{:S(2)}) collective-permute-start(f32[1,1024]{1,0:T(1,128)S(1)} %bitcast.5), channel_id=1, source_target_pairs={{0,2},{2,0},{1,3},{3,1},{4,6},{6,4},{5,7},{7,5},{8,10},{10,8},{9,1... | collective-permute-start | bytes 12296 | tf_op jit(solution)/shard_map/ppermute | solution.py:464
  18.0 1.7 %collective-permute-done.3.refs_4_.gain_ref = f32[1,1024]{1,0:T(1,128)S(1)} collective-permute-done((f32[1,1024]{1,0:T(1,128)S(1)}, f32[1,1024]{1,0:T(1,128)S(1)}, u32[]{:S(2)}, u32[]{:S(2)}) %collective-permute-start.3) | collective-permute-done | bytes 4128 | tf_op jit(solution)/shard_map/ppermute | solution.py:464
  19.7 0.0 collective-permute-done.refs_3_.q_sib_ref
  19.7 0.0 collective-permute-done.4.refs_0_
  19.7 1.3 %collective-permute-done.5.refs_1_ = s16[528,128]{1,0:T(8,128)(2,1)S(1)} collective-permute-done((s16[528,128]{1,0:T(8,128)(2,1)S(1)}, s16[528,128]{1,0:T(8,128)(2,1)S(1)}, u32[]{:S(2)}, u32[]{:S(2)}) %collective-permute-start.5) | collective-permute-done | bytes 135200 | tf_op jit(solution)/shard_map/ppermute | solution.py:464
  20.9 1.6 %collective-permute-done.6.refs_2_ = s16[528,128]{1,0:T(8,128)(2,1)S(1)} collective-permute-done((s16[528,128]{1,0:T(8,128)(2,1)S(1)}, s16[528,128]{1,0:T(8,128)(2,1)S(1)}, u32[]{:S(2)}, u32[]{:S(2)}) %collective-permute-start.6) | collective-permute-done | bytes 135200 | tf_op jit(solution)/shard_map/ppermute | solution.py:464
  22.5 0.1 level_states_0.1.refs_3_
  22.6 3.6 %collective-permute-start.12 = (s16[272,128]{1,0:T(8,128)(2,1)S(1)}, s16[272,128]{1,0:T(8,128)(2,1)S(1)}, u32[]{:S(2)}, u32[]{:S(2)}) collective-permute-start(s16[272,128]{1,0:T(8,128)(2,1)S(1)} %level_states_0.1.refs_3_), channel_id=1, source_target_pairs={{0,8},{8,16},{16,24},{1,9},{9,17},{17,25},{2,10},{10,18},{18,26},{... | collective-permute-start | bytes 208904 | tf_op jit(solution)/shard_map/ppermute | solution.py:471
  26.3 4.5 %collective-permute-start.11 = (s16[272,128]{1,0:T(8,128)(2,1)S(1)}, s16[272,128]{1,0:T(8,128)(2,1)S(1)}, u32[]{:S(2)}, u32[]{:S(2)}) collective-permute-start(s16[272,128]{1,0:T(8,128)(2,1)S(1)} %level_states_0.1.refs_3_), channel_id=1, source_target_pairs={{0,16},{8,24},{1,17},{9,25},{2,18},{10,26},{3,19},{11,27},{4,20},{... | collective-permute-start | bytes 208904 | tf_op jit(solution)/shard_map/ppermute | solution.py:471
  30.8 1.3 %collective-permute-start.10 = (s16[272,128]{1,0:T(8,128)(2,1)S(1)}, s16[272,128]{1,0:T(8,128)(2,1)S(1)}, u32[]{:S(2)}, u32[]{:S(2)}) collective-permute-start(s16[272,128]{1,0:T(8,128)(2,1)S(1)} %level_states_0.1.refs_3_), channel_id=1, source_target_pairs={{0,24},{1,25},{2,26},{3,27},{4,28},{5,29},{6,30},{7,31}} | collective-permute-start | bytes 208904 | tf_op jit(solution)/shard_map/ppermute | solution.py:471
  32.1 0.1 level_states_1.1.refs_6_
  32.2 1.3 %collective-permute-start.9 = (s16[272,128]{1,0:T(8,128)(2,1)S(1)}, s16[272,128]{1,0:T(8,128)(2,1)S(1)}, u32[]{:S(2)}, u32[]{:S(2)}) collective-permute-start(s16[272,128]{1,0:T(8,128)(2,1)S(1)} %level_states_1.1.refs_6_), channel_id=1, source_target_pairs={{0,8},{8,16},{16,24},{1,9},{9,17},{17,25},{2,10},{10,18},{18,26},{... | collective-permute-start | bytes 208904 | tf_op jit(solution)/shard_map/ppermute | solution.py:471
  33.5 1.3 %collective-permute-start.8 = (s16[272,128]{1,0:T(8,128)(2,1)S(1)}, s16[272,128]{1,0:T(8,128)(2,1)S(1)}, u32[]{:S(2)}, u32[]{:S(2)}) collective-permute-start(s16[272,128]{1,0:T(8,128)(2,1)S(1)} %level_states_1.1.refs_6_), channel_id=1, source_target_pairs={{0,16},{8,24},{1,17},{9,25},{2,18},{10,26},{3,19},{11,27},{4,20},{... | collective-permute-start | bytes 208904 | tf_op jit(solution)/shard_map/ppermute | solution.py:471
  34.8 0.0 collective-permute-done.12.refs_5_
  34.8 1.3 %collective-permute-start.7 = (s16[272,128]{1,0:T(8,128)(2,1)S(1)}, s16[272,128]{1,0:T(8,128)(2,1)S(1)}, u32[]{:S(2)}, u32[]{:S(2)}) collective-permute-start(s16[272,128]{1,0:T(8,128)(2,1)S(1)} %level_states_1.1.refs_6_), channel_id=1, source_target_pairs={{0,24},{1,25},{2,26},{3,27},{4,28},{5,29},{6,30},{7,31}} | collective-permute-start | bytes 208904 | tf_op jit(solution)/shard_map/ppermute | solution.py:471
  36.1 0.0 collective-permute-done.11.refs_4_
  36.1 0.0 collective-permute-done.10.refs_3_
  36.1 0.8 carries_0.1
  36.9 2.5 %collective-permute-start.14 = (s16[272,128]{1,0:T(8,128)(2,1)S(1)}, s16[272,128]{1,0:T(8,128)(2,1)S(1)}, u32[]{:S(2)}, u32[]{:S(2)}) collective-permute-start(s16[272,128]{1,0:T(8,128)(2,1)S(1)} %get-tuple-element.37), channel_id=1, source_target_pairs={{0,6},{2,4},{4,2},{6,0},{1,7},{3,5},{5,3},{7,1},{8,14},{10,12},{12... | collective-permute-start | bytes 208904 | tf_op jit(solution)/shard_map/ppermute | solution.py:464
  39.4 0.5 collective-permute-start.13
  39.9 0.0 collective-permute-done.9.refs_2_
  39.9 0.0 collective-permute-done.8.refs_1_
  39.9 0.0 collective-permute-done.7.refs_0_
  39.9 0.1 earlier_levels.1.refs_2_.refs_3_.refs_6_
  39.9 2.2 %collective-permute-done.14.refs_1_ = s16[272,128]{1,0:T(8,128)(2,1)S(1)} collective-permute-done((s16[272,128]{1,0:T(8,128)(2,1)S(1)}, s16[272,128]{1,0:T(8,128)(2,1)S(1)}, u32[]{:S(2)}, u32[]{:S(2)}) %collective-permute-start.14) | collective-permute-done | bytes 69664 | tf_op jit(solution)/shard_map/ppermute | solution.py:464
  42.1 1.5 %collective-permute-done.13.refs_0_ = s16[272,128]{1,0:T(8,128)(2,1)S(1)} collective-permute-done((s16[272,128]{1,0:T(8,128)(2,1)S(1)}, s16[272,128]{1,0:T(8,128)(2,1)S(1)}, u32[]{:S(2)}, u32[]{:S(2)}) %collective-permute-start.13) | collective-permute-done | bytes 69664 | tf_op jit(solution)/shard_map/ppermute | solution.py:464
  43.7 1.9 %attend_0_1_3.1.refs_4_ = bf16[512,512]{1,0:T(8,128)(2,1)S(1)} custom-call(s32[4]{0:T(128)S(1)} %pad_add_fusion.place_ref, bf16[256,2048]{1,0:T(8,128)(2,1)S(1)} %get-tuple-element.25.refs_0_.q_ref, bf16[256,2048]{1,0:T(8,128)(2,1)S(1)} %collective-permute-done.refs_3_.q_sib_ref, bf16[256,2048]{1,0:T(8,128)(2,1)S(1)} %get-tuple-element.27.k_ref, ...), custom_call_target="tpu_custom_call" | custom-call | flops 402653184 | bytes 2097152 | tf_op jit(solution)/shard_map/attend_0_1_3/pallas_call | solution.py:389
  45.6 0.8 collective-permute-start.17
  46.4 0.7 carries_1.1
  47.1 1.4 %collective-permute-start.16 = (s16[272,128]{1,0:T(8,128)(2,1)S(1)}, s16[272,128]{1,0:T(8,128)(2,1)S(1)}, u32[]{:S(2)}, u32[]{:S(2)}) collective-permute-start(s16[272,128]{1,0:T(8,128)(2,1)S(1)} %get-tuple-element.39), channel_id=1, source_target_pairs={{0,2},{2,0},{4,6},{6,4},{1,3},{3,1},{5,7},{7,5},{8,10},{10,8},{12,... | collective-permute-start | bytes 208904 | tf_op jit(solution)/shard_map/ppermute | solution.py:464
  48.4 1.2 %collective-permute-start.15 = (s16[272,128]{1,0:T(8,128)(2,1)S(1)}, s16[272,128]{1,0:T(8,128)(2,1)S(1)}, u32[]{:S(2)}, u32[]{:S(2)}) collective-permute-start(s16[272,128]{1,0:T(8,128)(2,1)S(1)} %get-tuple-element.38), channel_id=1, source_target_pairs={{0,6},{2,4},{4,2},{6,0},{1,7},{3,5},{5,3},{7,1},{8,14},{10,12},{12... | collective-permute-start | bytes 208904 | tf_op jit(solution)/shard_map/ppermute | solution.py:464
  49.7 9.8 %collective-permute-done.16.refs_0_ = s16[272,128]{1,0:T(8,128)(2,1)S(1)} collective-permute-done((s16[272,128]{1,0:T(8,128)(2,1)S(1)}, s16[272,128]{1,0:T(8,128)(2,1)S(1)}, u32[]{:S(2)}, u32[]{:S(2)}) %collective-permute-start.16) | collective-permute-done | bytes 69664 | tf_op jit(solution)/shard_map/ppermute | solution.py:464
  59.4 1.3 %attend_1_1.1.refs_1_ = bf16[512,256]{1,0:T(8,128)(2,1)S(1)} custom-call(s32[4]{0:T(128)S(1)} %pad_add_fusion.place_ref, bf16[256,2048]{1,0:T(8,128)(2,1)S(1)} %get-tuple-element.25.refs_0_.q_ref, bf16[256,2048]{1,0:T(8,128)(2,1)S(1)} %collective-permute-done.refs_3_.q_sib_ref, bf16[256,2048]{1,0:T(8,128)(2,1)S(1)} %get-tuple-element.27.k_ref, ...), custom_call_target="tpu_custom_call" | custom-call | flops 201326592 | bytes 1048576 | tf_op jit(solution)/shard_map/attend_1_1/pallas_call | solution.py:389
  60.8 1.1 %collective-permute-start.20 = (bf16[512,256]{1,0:T(8,128)(2,1)S(1)}, bf16[512,256]{1,0:T(8,128)(2,1)S(1)}, u32[]{:S(2)}, u32[]{:S(2)}) collective-permute-start(bf16[512,256]{1,0:T(8,128)(2,1)S(1)} %attend_1_1.1.refs_1_), channel_id=1, source_target_pairs={{0,2},{2,0},{1,3},{3,1},{4,6},{6,4},{5,7},{7,5},{8,10},{10,8},{9,1... | collective-permute-start | bytes 786440 | tf_op jit(solution)/shard_map/ppermute | solution.py:464
  61.8 0.0 collective-permute-done.15.refs_0_
  61.8 0.0 collective-permute-done.17.refs_2_
  61.8 1.3 %attend_1_3.1.refs_7_.refs_2_ = bf16[512,256]{1,0:T(8,128)(2,1)S(1)} custom-call(s32[4]{0:T(128)S(1)} %pad_add_fusion.place_ref, bf16[256,2048]{1,0:T(8,128)(2,1)S(1)} %get-tuple-element.25.refs_0_.q_ref, bf16[256,2048]{1,0:T(8,128)(2,1)S(1)} %collective-permute-done.refs_3_.q_sib_ref, bf16[256,2048]{1,0:T(8,128)(2,1)S(1)} %get-tuple-element.27.k_ref, ...), custom_call_target="tpu_custom_call" | custom-call | flops 201326592 | bytes 1048576 | tf_op jit(solution)/shard_map/attend_1_3/pallas_call | solution.py:389
  63.2 1.1 %own_carries.1 = (s16[528,128]{1,0:T(8,128)(2,1)S(1)}, s16[528,128]{1,0:T(8,128)(2,1)S(1)}, f32[2,2,128,128]{3,2,1,0:T(8,128)S(1)}, f32[2,2,128,128]{3,2,1,0:T(8,128)S(1)}) custom-call(s32[4]{0:T(128)S(1)} %pad_add_fusion.place_ref, f32[4,128,128]{2,1,0:T(8,128)S(1)} %get-tuple-element.32.own_ref, s16[528,128]{1,0:T(8,128)(2,1)S(1)} %collective-permute-done.4.refs_0_, ...), custom_call_target="tpu_custom_call" | custom-call | bytes 2621440 | tf_op jit(solution)/shard_map/own_carries/pallas_call | solution.py:331
  64.3 1.3 %collective-permute-start.21 = (f32[2,2,128,128]{3,2,1,0:T(8,128)S(1)}, f32[2,2,128,128]{3,2,1,0:T(8,128)S(1)}, u32[]{:S(2)}, u32[]{:S(2)}) collective-permute-start(f32[2,2,128,128]{3,2,1,0:T(8,128)S(1)} %get-tuple-element.43), channel_id=1, source_target_pairs={{0,4},{4,0},{1,5},{5,1},{2,6},{6,2},{3,7},{7,3},{8,12},{12,8},{9,1... | collective-permute-start | bytes 786440 | tf_op jit(solution)/shard_map/ppermute | solution.py:464
  65.5 0.8 %collective-permute-start.18 = (bf16[512,256]{1,0:T(8,128)(2,1)S(1)}, bf16[512,256]{1,0:T(8,128)(2,1)S(1)}, u32[]{:S(2)}, u32[]{:S(2)}) collective-permute-start(bf16[512,256]{1,0:T(8,128)(2,1)S(1)} %attend_1_3.1.refs_7_.refs_2_), channel_id=1, source_target_pairs={{0,2},{2,0},{1,3},{3,1},{4,6},{6,4},{5,7},{7,5},{8,10},{10,8},{9,1... | collective-permute-start | bytes 786440 | tf_op jit(solution)/shard_map/ppermute | solution.py:464
  66.3 1.1 %collective-permute-start.19 = (s16[528,128]{1,0:T(8,128)(2,1)S(1)}, s16[528,128]{1,0:T(8,128)(2,1)S(1)}, u32[]{:S(2)}, u32[]{:S(2)}) collective-permute-start(s16[528,128]{1,0:T(8,128)(2,1)S(1)} %get-tuple-element.41), channel_id=1, source_target_pairs={{0,4},{2,6},{4,0},{6,2},{1,5},{3,7},{5,1},{7,3},{8,12},{10,14},{12... | collective-permute-start | bytes 405512 | tf_op jit(solution)/shard_map/ppermute | solution.py:464
  67.4 4.8 %collective-permute-done.19.refs_1_ = s16[528,128]{1,0:T(8,128)(2,1)S(1)} collective-permute-done((s16[528,128]{1,0:T(8,128)(2,1)S(1)}, s16[528,128]{1,0:T(8,128)(2,1)S(1)}, u32[]{:S(2)}, u32[]{:S(2)}) %collective-permute-start.19) | collective-permute-done | bytes 135200 | tf_op jit(solution)/shard_map/ppermute | solution.py:464
  72.2 1.9 %attend_0_0_2.1.refs_2_.refs_0_ = bf16[512,512]{1,0:T(8,128)(2,1)S(1)} custom-call(s32[4]{0:T(128)S(1)} %pad_add_fusion.place_ref, bf16[256,2048]{1,0:T(8,128)(2,1)S(1)} %get-tuple-element.25.refs_0_.q_ref, bf16[256,2048]{1,0:T(8,128)(2,1)S(1)} %collective-permute-done.refs_3_.q_sib_ref, bf16[256,2048]{1,0:T(8,128)(2,1)S(1)} %get-tuple-element.27.k_ref, ...), custom_call_target="tpu_custom_call" | custom-call | flops 402653184 | bytes 2097152 | tf_op jit(solution)/shard_map/attend_0_0_2/pallas_call | solution.py:389
  74.0 1.9 %attend_1_0_2.1.refs_1_ = bf16[512,512]{1,0:T(8,128)(2,1)S(1)} custom-call(s32[4]{0:T(128)S(1)} %pad_add_fusion.place_ref, bf16[256,2048]{1,0:T(8,128)(2,1)S(1)} %get-tuple-element.25.refs_0_.q_ref, bf16[256,2048]{1,0:T(8,128)(2,1)S(1)} %collective-permute-done.refs_3_.q_sib_ref, bf16[256,2048]{1,0:T(8,128)(2,1)S(1)} %get-tuple-element.27.k_ref, ...), custom_call_target="tpu_custom_call" | custom-call | flops 402653184 | bytes 2097152 | tf_op jit(solution)/shard_map/attend_1_0_2/pallas_call | solution.py:389
  75.9 0.0 collective-permute-done.20.refs_3_
  75.9 1.8 %assemble.1.refs_1_ = bf16[1024,1024]{1,0:T(8,128)(2,1)} custom-call(s32[4]{0:T(128)S(1)} %pad_add_fusion.place_ref, bf16[512,512]{1,0:T(8,128)(2,1)S(1)} %attend_0_0_2.1.refs_2_.refs_0_, bf16[512,512]{1,0:T(8,128)(2,1)S(1)} %attend_1_0_2.1.refs_1_, bf16[512,512]{1,0:T(8,128)(2,1)S(1)} %collective-permute-done.17.refs_2_, ...), custom_call_target="tpu_custom_call" | custom-call | tf_op jit(solution)/shard_map/assemble/pallas_call | solution.py:428
  77.8 0.0 collective-permute-done.21.refs_1_
  77.8 1.4 %assemble_cache.1 = f32[1,8,128,128]{3,2,1,0:T(8,128)} custom-call(s32[4]{0:T(128)S(1)} %pad_add_fusion.place_ref, f32[2,2,128,128]{3,2,1,0:T(8,128)S(1)} %get-tuple-element.42.refs_0_, f32[2,2,128,128]{3,2,1,0:T(8,128)S(1)} %collective-permute-done.21.refs_1_), custom_call_target="tpu_custom_call" | custom-call | tf_op jit(solution)/shard_map/assemble_cache/pallas_call | solution.py:449
  79.1 0.0 collective-permute-done.18.refs_0_
  79.1 1.3 %finish.1 = bf16[1024,1024]{1,0:T(8,128)(2,1)} custom-call(s32[4]{0:T(128)S(1)} %pad_add_fusion.place_ref, bf16[512,256]{1,0:T(8,128)(2,1)S(1)} %collective-permute-done.18.refs_0_, bf16[1024,1024]{1,0:T(8,128)(2,1)} %assemble.1.refs_1_), custom_call_target="tpu_custom_call", output_to_operand_aliasing={{}: (2, {})} | custom-call | tf_op jit(solution)/shard_map/finish/pallas_call | solution.py:428
  (2 shorter events, 0.0 us)
Async XLA Ops:
  0.7 5.0 %copy-start = (bf16[256,4096]{1,0:T(8,128)(2,1)S(1)}, bf16[256,4096]{1,0:T(8,128)(2,1)}, u32[]{:S(2)}) copy-start(bf16[256,4096]{1,0:T(8,128)(2,1)} %queries_ref.1) | copy-start | bytes 6291460
  5.1 2.8 %collective-permute-start.1 = (bf16[256,2048]{1,0:T(8,128)(2,1)S(1)}, bf16[256,2048]{1,0:T(8,128)(2,1)S(1)}, u32[]{:S(2)}, u32[]{:S(2)}) collective-permute-start(bf16[256,2048]{1,0:T(8,128)(2,1)S(1)} %get-tuple-element.28), channel_id=1, source_target_pairs={{0,1},{1,0},{2,3},{3,2},{4,5},{5,4},{6,7},{7,6},{8,9},{9,8},{10,11... | collective-permute-start | bytes 3145736 | tf_op jit(solution)/shard_map/ppermute | solution.py:464
  5.6 3.8 %collective-permute-start.2 = (bf16[256,2048]{1,0:T(8,128)(2,1)S(1)}, bf16[256,2048]{1,0:T(8,128)(2,1)S(1)}, u32[]{:S(2)}, u32[]{:S(2)}) collective-permute-start(bf16[256,2048]{1,0:T(8,128)(2,1)S(1)} %get-tuple-element.30), channel_id=1, source_target_pairs={{0,1},{1,0},{2,3},{3,2},{4,5},{5,4},{6,7},{7,6},{8,9},{9,8},{10,11... | collective-permute-start | bytes 3145736 | tf_op jit(solution)/shard_map/ppermute | solution.py:464
  6.4 13.2 %collective-permute-start = (bf16[256,2048]{1,0:T(8,128)(2,1)S(1)}, bf16[256,2048]{1,0:T(8,128)(2,1)S(1)}, u32[]{:S(2)}, u32[]{:S(2)}) collective-permute-start(bf16[256,2048]{1,0:T(8,128)(2,1)S(1)} %get-tuple-element.26), channel_id=1, source_target_pairs={{0,1},{1,0},{2,3},{3,2},{4,5},{5,4},{6,7},{7,6},{8,9},{9,8},{10,11... | collective-permute-start | bytes 3145736 | tf_op jit(solution)/shard_map/ppermute | solution.py:464
  9.4 6.6 %copy-start.1 = (f32[1024]{0:T(1024)S(1)}, f32[1024]{0:T(1024)}, u32[]{:S(2)}) copy-start(f32[1024]{0:T(1024)} %param.9) | copy-start | bytes 12292
  11.5 8.2 %collective-permute-start.4 = (s16[528,128]{1,0:T(8,128)(2,1)S(1)}, s16[528,128]{1,0:T(8,128)(2,1)S(1)}, u32[]{:S(2)}, u32[]{:S(2)}) collective-permute-start(s16[528,128]{1,0:T(8,128)(2,1)S(1)} %get-tuple-element.33), channel_id=1, source_target_pairs={{0,2},{2,0},{4,6},{6,4},{1,3},{3,1},{5,7},{7,5},{8,10},{10,8},{12,... | collective-permute-start | bytes 405512 | tf_op jit(solution)/shard_map/ppermute | solution.py:464
  14.5 6.5 %collective-permute-start.5 = (s16[528,128]{1,0:T(8,128)(2,1)S(1)}, s16[528,128]{1,0:T(8,128)(2,1)S(1)}, u32[]{:S(2)}, u32[]{:S(2)}) collective-permute-start(s16[528,128]{1,0:T(8,128)(2,1)S(1)} %get-tuple-element.34), channel_id=1, source_target_pairs={{0,4},{2,6},{4,0},{6,2},{1,5},{3,7},{5,1},{7,3},{8,12},{10,14},{12... | collective-permute-start | bytes 405512 | tf_op jit(solution)/shard_map/ppermute | solution.py:464
  16.0 6.6 %collective-permute-start.6 = (s16[528,128]{1,0:T(8,128)(2,1)S(1)}, s16[528,128]{1,0:T(8,128)(2,1)S(1)}, u32[]{:S(2)}, u32[]{:S(2)}) collective-permute-start(s16[528,128]{1,0:T(8,128)(2,1)S(1)} %get-tuple-element.35), channel_id=1, source_target_pairs={{0,6},{2,4},{4,2},{6,0},{1,7},{3,5},{5,3},{7,1},{8,14},{10,12},{12... | collective-permute-start | bytes 405512 | tf_op jit(solution)/shard_map/ppermute | solution.py:464
  16.0 3.6 %collective-permute-start.3 = (f32[1,1024]{1,0:T(1,128)S(1)}, f32[1,1024]{1,0:T(1,128)S(1)}, u32[]{:S(2)}, u32[]{:S(2)}) collective-permute-start(f32[1,1024]{1,0:T(1,128)S(1)} %bitcast.5), channel_id=1, source_target_pairs={{0,2},{2,0},{1,3},{3,1},{4,6},{6,4},{5,7},{7,5},{8,10},{10,8},{9,1... | collective-permute-start | bytes 12296 | tf_op jit(solution)/shard_map/ppermute | solution.py:464
  22.6 12.2 %collective-permute-start.12 = (s16[272,128]{1,0:T(8,128)(2,1)S(1)}, s16[272,128]{1,0:T(8,128)(2,1)S(1)}, u32[]{:S(2)}, u32[]{:S(2)}) collective-permute-start(s16[272,128]{1,0:T(8,128)(2,1)S(1)} %level_states_0.1.refs_3_), channel_id=1, source_target_pairs={{0,8},{8,16},{16,24},{1,9},{9,17},{17,25},{2,10},{10,18},{18,26},{... | collective-permute-start | bytes 208904 | tf_op jit(solution)/shard_map/ppermute | solution.py:471
  26.3 9.8 %collective-permute-start.11 = (s16[272,128]{1,0:T(8,128)(2,1)S(1)}, s16[272,128]{1,0:T(8,128)(2,1)S(1)}, u32[]{:S(2)}, u32[]{:S(2)}) collective-permute-start(s16[272,128]{1,0:T(8,128)(2,1)S(1)} %level_states_0.1.refs_3_), channel_id=1, source_target_pairs={{0,16},{8,24},{1,17},{9,25},{2,18},{10,26},{3,19},{11,27},{4,20},{... | collective-permute-start | bytes 208904 | tf_op jit(solution)/shard_map/ppermute | solution.py:471
  30.8 5.3 %collective-permute-start.10 = (s16[272,128]{1,0:T(8,128)(2,1)S(1)}, s16[272,128]{1,0:T(8,128)(2,1)S(1)}, u32[]{:S(2)}, u32[]{:S(2)}) collective-permute-start(s16[272,128]{1,0:T(8,128)(2,1)S(1)} %level_states_0.1.refs_3_), channel_id=1, source_target_pairs={{0,24},{1,25},{2,26},{3,27},{4,28},{5,29},{6,30},{7,31}} | collective-permute-start | bytes 208904 | tf_op jit(solution)/shard_map/ppermute | solution.py:471
  32.2 7.7 %collective-permute-start.9 = (s16[272,128]{1,0:T(8,128)(2,1)S(1)}, s16[272,128]{1,0:T(8,128)(2,1)S(1)}, u32[]{:S(2)}, u32[]{:S(2)}) collective-permute-start(s16[272,128]{1,0:T(8,128)(2,1)S(1)} %level_states_1.1.refs_6_), channel_id=1, source_target_pairs={{0,8},{8,16},{16,24},{1,9},{9,17},{17,25},{2,10},{10,18},{18,26},{... | collective-permute-start | bytes 208904 | tf_op jit(solution)/shard_map/ppermute | solution.py:471
  33.5 6.4 %collective-permute-start.8 = (s16[272,128]{1,0:T(8,128)(2,1)S(1)}, s16[272,128]{1,0:T(8,128)(2,1)S(1)}, u32[]{:S(2)}, u32[]{:S(2)}) collective-permute-start(s16[272,128]{1,0:T(8,128)(2,1)S(1)} %level_states_1.1.refs_6_), channel_id=1, source_target_pairs={{0,16},{8,24},{1,17},{9,25},{2,18},{10,26},{3,19},{11,27},{4,20},{... | collective-permute-start | bytes 208904 | tf_op jit(solution)/shard_map/ppermute | solution.py:471
  34.8 5.1 %collective-permute-start.7 = (s16[272,128]{1,0:T(8,128)(2,1)S(1)}, s16[272,128]{1,0:T(8,128)(2,1)S(1)}, u32[]{:S(2)}, u32[]{:S(2)}) collective-permute-start(s16[272,128]{1,0:T(8,128)(2,1)S(1)} %level_states_1.1.refs_6_), channel_id=1, source_target_pairs={{0,24},{1,25},{2,26},{3,27},{4,28},{5,29},{6,30},{7,31}} | collective-permute-start | bytes 208904 | tf_op jit(solution)/shard_map/ppermute | solution.py:471
  36.9 5.3 %collective-permute-start.14 = (s16[272,128]{1,0:T(8,128)(2,1)S(1)}, s16[272,128]{1,0:T(8,128)(2,1)S(1)}, u32[]{:S(2)}, u32[]{:S(2)}) collective-permute-start(s16[272,128]{1,0:T(8,128)(2,1)S(1)} %get-tuple-element.37), channel_id=1, source_target_pairs={{0,6},{2,4},{4,2},{6,0},{1,7},{3,5},{5,3},{7,1},{8,14},{10,12},{12... | collective-permute-start | bytes 208904 | tf_op jit(solution)/shard_map/ppermute | solution.py:464
  39.4 4.3 %collective-permute-start.13 = (s16[272,128]{1,0:T(8,128)(2,1)S(1)}, s16[272,128]{1,0:T(8,128)(2,1)S(1)}, u32[]{:S(2)}, u32[]{:S(2)}) collective-permute-start(s16[272,128]{1,0:T(8,128)(2,1)S(1)} %get-tuple-element.36.refs_3_), channel_id=1, source_target_pairs={{0,2},{2,0},{4,6},{6,4},{1,3},{3,1},{5,7},{7,5},{8,10},{10,8},{12,... | collective-permute-start | bytes 208904 | tf_op jit(solution)/shard_map/ppermute | solution.py:464
  45.6 16.3 %collective-permute-start.17 = (bf16[512,512]{1,0:T(8,128)(2,1)S(1)}, bf16[512,512]{1,0:T(8,128)(2,1)S(1)}, u32[]{:S(2)}, u32[]{:S(2)}) collective-permute-start(bf16[512,512]{1,0:T(8,128)(2,1)S(1)} %attend_0_1_3.1.refs_4_), channel_id=1, source_target_pairs={{0,2},{2,0},{1,3},{3,1},{4,6},{6,4},{5,7},{7,5},{8,10},{10,8},{9,1... | collective-permute-start | bytes 1572872 | tf_op jit(solution)/shard_map/ppermute | solution.py:464
  47.1 12.4 %collective-permute-start.16 = (s16[272,128]{1,0:T(8,128)(2,1)S(1)}, s16[272,128]{1,0:T(8,128)(2,1)S(1)}, u32[]{:S(2)}, u32[]{:S(2)}) collective-permute-start(s16[272,128]{1,0:T(8,128)(2,1)S(1)} %get-tuple-element.39), channel_id=1, source_target_pairs={{0,2},{2,0},{4,6},{6,4},{1,3},{3,1},{5,7},{7,5},{8,10},{10,8},{12,... | collective-permute-start | bytes 208904 | tf_op jit(solution)/shard_map/ppermute | solution.py:464
  48.4 13.4 %collective-permute-start.15 = (s16[272,128]{1,0:T(8,128)(2,1)S(1)}, s16[272,128]{1,0:T(8,128)(2,1)S(1)}, u32[]{:S(2)}, u32[]{:S(2)}) collective-permute-start(s16[272,128]{1,0:T(8,128)(2,1)S(1)} %get-tuple-element.38), channel_id=1, source_target_pairs={{0,6},{2,4},{4,2},{6,0},{1,7},{3,5},{5,3},{7,1},{8,14},{10,12},{12... | collective-permute-start | bytes 208904 | tf_op jit(solution)/shard_map/ppermute | solution.py:464
  60.8 15.1 %collective-permute-start.20 = (bf16[512,256]{1,0:T(8,128)(2,1)S(1)}, bf16[512,256]{1,0:T(8,128)(2,1)S(1)}, u32[]{:S(2)}, u32[]{:S(2)}) collective-permute-start(bf16[512,256]{1,0:T(8,128)(2,1)S(1)} %attend_1_1.1.refs_1_), channel_id=1, source_target_pairs={{0,2},{2,0},{1,3},{3,1},{4,6},{6,4},{5,7},{7,5},{8,10},{10,8},{9,1... | collective-permute-start | bytes 786440 | tf_op jit(solution)/shard_map/ppermute | solution.py:464
  64.3 13.5 %collective-permute-start.21 = (f32[2,2,128,128]{3,2,1,0:T(8,128)S(1)}, f32[2,2,128,128]{3,2,1,0:T(8,128)S(1)}, u32[]{:S(2)}, u32[]{:S(2)}) collective-permute-start(f32[2,2,128,128]{3,2,1,0:T(8,128)S(1)} %get-tuple-element.43), channel_id=1, source_target_pairs={{0,4},{4,0},{1,5},{5,1},{2,6},{6,2},{3,7},{7,3},{8,12},{12,8},{9,1... | collective-permute-start | bytes 786440 | tf_op jit(solution)/shard_map/ppermute | solution.py:464
  65.5 13.6 %collective-permute-start.18 = (bf16[512,256]{1,0:T(8,128)(2,1)S(1)}, bf16[512,256]{1,0:T(8,128)(2,1)S(1)}, u32[]{:S(2)}, u32[]{:S(2)}) collective-permute-start(bf16[512,256]{1,0:T(8,128)(2,1)S(1)} %attend_1_3.1.refs_7_.refs_2_), channel_id=1, source_target_pairs={{0,2},{2,0},{1,3},{3,1},{4,6},{6,4},{5,7},{7,5},{8,10},{10,8},{9,1... | collective-permute-start | bytes 786440 | tf_op jit(solution)/shard_map/ppermute | solution.py:464
  66.3 5.8 %collective-permute-start.19 = (s16[528,128]{1,0:T(8,128)(2,1)S(1)}, s16[528,128]{1,0:T(8,128)(2,1)S(1)}, u32[]{:S(2)}, u32[]{:S(2)}) collective-permute-start(s16[528,128]{1,0:T(8,128)(2,1)S(1)} %get-tuple-element.41), channel_id=1, source_target_pairs={{0,4},{2,6},{4,0},{6,2},{1,5},{3,7},{5,1},{7,3},{8,12},{10,14},{12... | collective-permute-start | bytes 405512 | tf_op jit(solution)/shard_map/ppermute | solution.py:464

commit v7 on v5

--- a/solution.py
+++ b/solution.py
@@ -167,6 +167,14 @@
 
 def plus(left, right):
     return [a + b for a, b in zip(left, right)]
+
+
+def total_of(refs, each):
+    total = [jnp.zeros((HD, HD), jnp.float32)] * each
+    for ref in refs:
+        coded = ref.dtype == jnp.int16
+        total = plus(total, decoded(ref) if coded else [ref[i] for i in range(each)])
+    return total
 
 
 def coded_shape(heads):
@@ -219,10 +227,7 @@
 
 def level_states(plan, own, others, half, after):
     def kernel(own_ref, *refs):
-        total = [own_ref[i] for i in range(plan.each)]
-        for ref in refs[: len(others)]:
-            total = plus(total, decoded(ref))
-        code(total, refs[-1])
+        code(total_of((own_ref, *refs[: len(others)]), plan.each), refs[-1])
 
     return pl.pallas_call(
         kernel,
@@ -238,9 +243,7 @@
 def carried(plan, place_ref, own, others, levels, offsets):
     x, y = place_ref[1], place_ref[2]
     here = x * plan.n_y + y
-    earlier = [jnp.zeros((HD, HD), jnp.float32)] * plan.each
-    for ref in levels:
-        earlier = plus(earlier, decoded(ref))
+    earlier = total_of(levels, plan.each)
     states = [[own[i] for i in range(plan.each)]] + [decoded(ref) for ref in others]
 
     def add(totals, keep_of):
@@ -279,14 +282,15 @@
 
 
 def own_carries(plan, place, own, others, levels, offsets, after):
-    n_others, n_levels = len(others[0]), len(levels[0])
-    each_half = 1 + n_others + n_levels
+    n_others = len(others[0])
+    operands = [(own[h], *others[h], *levels[h]) for h in range(plan.halves)]
+    starts = [sum(map(len, operands[:h])) for h in range(plan.halves + 1)]
 
     def kernel(place_ref, *refs):
-        outs = refs[plan.halves * each_half + len(after) :]
+        outs = refs[starts[-1] + len(after) :]
         befores = [[] for _ in offsets]
         for half in range(plan.halves):
-            own_ref, *of_half = refs[half * each_half : (half + 1) * each_half]
+            own_ref, *of_half = refs[starts[half] : starts[half + 1]]
             before, blocks = carried(
                 plan, place_ref, own_ref, of_half[:n_others], of_half[n_others:], offsets
             )
@@ -300,17 +304,16 @@
         for states, ref in zip(befores, outs):
             code(states, ref)
 
-    operands = [a for h in range(plan.halves) for a in (own[h], *others[h], *levels[h])]
     return pl.pallas_call(
         kernel,
         out_shape=[coded_shape(plan.halves * plan.each)] * len(offsets)
         + [states_shape(plan.halves, plan.each)] * plan.n_inner,
-        in_specs=[SMEM] + [VMEM] * len(operands) + [ANY] * len(after),
+        in_specs=[SMEM] + [VMEM] * starts[-1] + [ANY] * len(after),
         out_specs=[VMEM] * (len(offsets) + plan.n_inner),
         compiler_params=params(),
-        cost_estimate=cost(0, (plan.plane * 4 + n_levels) * plan.each * HD * HD * 4),
+        cost_estimate=cost(0, plan.plane * plan.each * HD * HD * 20),
         name="own_carries",
-    )(place, *operands, *after)
+    )(place, *[a for arrays in operands for a in arrays], *after)
 
 
 def attend(plan, place, query, key, value, carry, first, gain, half, offsets, after=()):
@@ -489,26 +492,26 @@
 
     def send_stage(half, carry, after):
         for y in range(1, plan.n_y):
-            group = of_group[y]
-            pieces = [group[:-1], group[-1:]] if half and len(group) > 1 else [group]
-            for offsets in pieces:
-                arrived = [a for a, h, os in parts if h == 0 and offsets == group[-1:] and os == group]
-                part = part_of(half, offsets, carry, after + arrived)
-                parts.append((swap(part, "y", y, plan.n_y), half, offsets))
-                after = [part]
+            part = part_of(half, of_group[y], carry, after)
+            parts.append((swap(part, "y", y, plan.n_y), half, of_group[y]))
+            after = [part]
         return after
 
-    owner_stage(0, [query[0]])
-    level_stage(0, gains[1:])
-    if plan.halves > 1:
-        owner_stage(1, [coded[0], query[1]])
-    done, carry = carry_stage(0, [own[-1]])
-    if plan.halves > 1:
-        level_stage(1, [done])
-    after = send_stage(0, carry, [coded[-1]])
-    if plan.halves > 1:
-        _, carry = carry_stage(1, after)
-        after = send_stage(1, carry, [])
+    after = [query[0]]
+    for half in halves:
+        owner_stage(half, after)
+        after = [own[-1], query[1]]
+    for half in halves:
+        level_stage(half, after)
+        after = [coded[-1]]
+    carry = []
+    after = [*after, *gains[1:]]
+    for half in halves:
+        done, of_half = carry_stage(half, after)
+        carry.append(of_half)
+        after = [done]
+    for half in halves:
+        after = send_stage(half, carry[half], after)
     sends = own_carries(plan, place, own, others, levels, of_group[0], after)
     own_carry = {o: in_level(a, o) if o else a for o, a in zip(of_group[0], sends)}
     caches = [

time: 80.4 us -> 69.5 us (0.86)
  waiting for transfers between devices: 18.9 us -> 13.2 us
  starting transfers between devices: 37 us -> 32.5 us
    ppermute x19 -> x18, waiting for transfers between devices: 17 us -> 13.2 us  [swap(): return lax.ppermute(array, axes, [(i, i ^ offset) for i in range(size)])]
    ppermute x6, starting transfers between devices: 16.1 us -> 13 us  [to_later(): return lax.ppermute(array, 'outer', pairs)]
    ppermute x6, waiting for transfers between devices: 1.92 us -> 0.02 us  [to_later(): return lax.ppermute(array, 'outer', pairs)]
    ppermute x19 -> x18, starting transfers between devices: 20.9 us -> 19.6 us  [swap(): return lax.ppermute(array, axes, [(i, i ^ offset) for i in range(size)])]
    pallas_call x5 -> x4, Pallas kernels: 8.28 us -> 7.47 us  [attend(): pl.pallas_call(kernel, out_shape=jax.ShapeDtypeStruct((CORES * rows, head...]
  transfers between devices with their start and end apart: 25 -> 24, of which waited for: 11 -> 8; matrix products, arithmetic and copies ran while one was open for 0% -> 0% of each run, Pallas kernels for 20% -> 24%
where the time goes in v7:
time: 69.5 us; the launch traced here: 69.3 us
  starting transfers between devices  32.5 us (47%)
  Pallas kernels  22.6 us (33%)
  waiting for transfers between devices  13.2 us (19%)
  between operations  0.85 us (1%)
    ppermute x18, starting transfers between devices, swap(): return lax.ppermute(array, axes, [(i, i ^ offset) for i in range(size)])  19.6 us
    ppermute x18, waiting for transfers between devices, swap(): return lax.ppermute(array, axes, [(i, i ^ offset) for i in range(size)])  13.2 us
    ppermute x6, starting transfers between devices, to_later(): return lax.ppermute(array, 'outer', pairs)  13 us
    pallas_call x4, Pallas kernels, attend(): pl.pallas_call(kernel, out_shape=jax.ShapeDtypeStruct((CORES * rows, head...  7.47 us
    pallas_call x1, Pallas kernels, decode(): pl.pallas_call(kernel, out_shape=[jax.ShapeDtypeStruct((rows, plan.n_y *...  4.36 us
    pallas_call x2, Pallas kernels, assemble(): pl.pallas_call(kernel, out_shape=jax.ShapeDtypeStruct((plan.n_y * rows, p...  3.08 us
    pallas_call x2, Pallas kernels, chunk_states(): pl.pallas_call(kernel, out_shape=[states_shape(plan.each), states_shape(p...  2.73 us
    pallas_call x2, Pallas kernels, carries(): pl.pallas_call(kernel, out_shape=[coded_shape(plan.each)] * len(offsets),...  1.5 us
  transfers between devices with their start and end apart: 24, of which 8 were waited for; matrix products, arithmetic and copies ran while one was open for 0% of the time, Pallas kernels for 24%

profile of v7, /device:TPU:0, one launch (start us, length us, event | category | flops | bytes accessed | tf_op | source)
XLA Modules:
  0.0 69.3 jit_solution(9604378976089405142)
XLA Ops:
  0.6 0.1 pad_add_fusion.place_ref
  0.7 4.4 %decode.1 = (bf16[256,2048]{1,0:T(8,128)(2,1)S(1)}, bf16[256,2048]{1,0:T(8,128)(2,1)S(1)}, bf16[256,2048]{1,0:T(8,128)(2,1)S(1)}, bf16[256,2048]{1,0:T(8,128)(2,...) custom-call(s32[4]{0:T(128)S(1)} %pad_add_fusion.place_ref, s32[256,4096]{1,0:T(8,128)} %refs_0_.1, ...), custom_call_target="tpu_custom_call" | custom-call | flops 4194304 | bytes 14680064 | tf_op jit(solution)/shard_map/decode/pallas_call | solution.py:100
  5.1 0.5 collective-permute-start.1
  5.6 0.1 collective-permute-start.2
  5.7 0.8 %spike_queries.1 = (bf16[256,2048]{1,0:T(8,128)(2,1)S(1)}, bf16[256,2048]{1,0:T(8,128)(2,1)S(1)}) custom-call(s32[4]{0:T(128)S(1)} %pad_add_fusion.place_ref, bf16[256,4096]{1,0:T(8,128)(2,1)S(1)} %copy-done, bf16[256,2048]{1,0:T(8,128)(2,1)S(1)} %get-tuple-element.28.refs_0_, bf16[256,2048]{1,0:T(8,128)(2,1)S(1)} %get-tuple-element.29.refs_1_), custom_call_target="tpu_custom_call" | custom-call | flops 1048576 | bytes 6291456 | tf_op jit(solution)/shard_map/spike_queries/pallas_call | solution.py:122
  6.4 0.5 collective-permute-start
  6.9 0.9 %collective-permute-done.1.k_sib_ref = bf16[256,2048]{1,0:T(8,128)(2,1)S(1)} collective-permute-done((bf16[256,2048]{1,0:T(8,128)(2,1)S(1)}, bf16[256,2048]{1,0:T(8,128)(2,1)S(1)}, u32[]{:S(2)}, u32[]{:S(2)}) %collective-permute-start.1) | collective-permute-done | bytes 1048608 | tf_op jit(solution)/shard_map/ppermute | solution.py:440
  7.9 1.5 %collective-permute-done.2.v_sib_ref = bf16[256,2048]{1,0:T(8,128)(2,1)S(1)} collective-permute-done((bf16[256,2048]{1,0:T(8,128)(2,1)S(1)}, bf16[256,2048]{1,0:T(8,128)(2,1)S(1)}, u32[]{:S(2)}, u32[]{:S(2)}) %collective-permute-start.2) | collective-permute-done | bytes 1048608 | tf_op jit(solution)/shard_map/ppermute | solution.py:440
  9.4 1.4 %chunk_states_0.1 = (f32[2,128,128]{2,1,0:T(8,128)S(1)}, f32[4,2,128,128]{3,2,1,0:T(8,128)S(1)}, s16[272,128]{1,0:T(8,128)(2,1)S(1)}, s16[272,128]{1,0:T(8,128)(2,1)S(1)}, s16[272,128]{1,0:T(8,128)(2,1)S(1)}) custom-call(s32[4]{0:T(128)S(1)} %pad_add_fusion.place_ref, bf16[256,2048]{1,0:T(8,128)(2,1)S(1)} %get-tuple-element.32.k_ref, ...), custom_call_target="tpu_custom_call" | custom-call | flops 134217728 | bytes 2883584 | tf_op jit(solution)/shard_map/chunk_states_0/pallas_call | solution.py:214
  10.8 3.0 %collective-permute-start.7 = (s16[272,128]{1,0:T(8,128)(2,1)S(1)}, s16[272,128]{1,0:T(8,128)(2,1)S(1)}, u32[]{:S(2)}, u32[]{:S(2)}) collective-permute-start(s16[272,128]{1,0:T(8,128)(2,1)S(1)} %get-tuple-element.42), channel_id=1, source_target_pairs={{0,2},{2,0},{4,6},{6,4},{1,3},{3,1},{5,7},{7,5},{8,10},{10,8},{12,... | collective-permute-start | bytes 208904 | tf_op jit(solution)/shard_map/ppermute | solution.py:440
  13.7 1.5 %collective-permute-start.8 = (s16[272,128]{1,0:T(8,128)(2,1)S(1)}, s16[272,128]{1,0:T(8,128)(2,1)S(1)}, u32[]{:S(2)}, u32[]{:S(2)}) collective-permute-start(s16[272,128]{1,0:T(8,128)(2,1)S(1)} %get-tuple-element.43), channel_id=1, source_target_pairs={{0,4},{2,6},{4,0},{6,2},{1,5},{3,7},{5,1},{7,3},{8,12},{10,14},{12... | collective-permute-start | bytes 208904 | tf_op jit(solution)/shard_map/ppermute | solution.py:440
  15.2 0.0 collective-permute-start.9
  15.3 0.0 collective-permute-done.refs_1_.refs_4_.q_sib_ref
  15.3 1.4 %chunk_states_1.1 = (f32[2,128,128]{2,1,0:T(8,128)S(1)}, f32[4,2,128,128]{3,2,1,0:T(8,128)S(1)}, s16[272,128]{1,0:T(8,128)(2,1)S(1)}, s16[272,128]{1,0:T(8,128)(2,1)S(1)}, s16[272,128]{1,0:T(8,128)(2,1)S(1)}) custom-call(s32[4]{0:T(128)S(1)} %pad_add_fusion.place_ref, bf16[256,2048]{1,0:T(8,128)(2,1)S(1)} %get-tuple-element.32.k_ref, ...), custom_call_target="tpu_custom_call" | custom-call | flops 134217728 | bytes 2883584 | tf_op jit(solution)/shard_map/chunk_states_1/pallas_call | solution.py:214
  16.6 2.0 %collective-permute-start.4 = (s16[272,128]{1,0:T(8,128)(2,1)S(1)}, s16[272,128]{1,0:T(8,128)(2,1)S(1)}, u32[]{:S(2)}, u32[]{:S(2)}) collective-permute-start(s16[272,128]{1,0:T(8,128)(2,1)S(1)} %get-tuple-element.39), channel_id=1, source_target_pairs={{0,2},{2,0},{4,6},{6,4},{1,3},{3,1},{5,7},{7,5},{8,10},{10,8},{12,... | collective-permute-start | bytes 208904 | tf_op jit(solution)/shard_map/ppermute | solution.py:440
  18.6 1.5 %collective-permute-start.5 = (s16[272,128]{1,0:T(8,128)(2,1)S(1)}, s16[272,128]{1,0:T(8,128)(2,1)S(1)}, u32[]{:S(2)}, u32[]{:S(2)}) collective-permute-start(s16[272,128]{1,0:T(8,128)(2,1)S(1)} %get-tuple-element.40), channel_id=1, source_target_pairs={{0,4},{2,6},{4,0},{6,2},{1,5},{3,7},{5,1},{7,3},{8,12},{10,14},{12... | collective-permute-start | bytes 208904 | tf_op jit(solution)/shard_map/ppermute | solution.py:440
  20.1 0.0 collective-permute-done.7.refs_0_.refs_1_
  20.1 0.0 collective-permute-start.6
  20.2 0.0 collective-permute-done.8.refs_1_.refs_2_
  20.2 0.7 collective-permute-done.9.refs_2_.refs_3_
  20.9 0.1 level_states_0.1.refs_3_
  21.0 3.3 %collective-permute-start.15 = (s16[272,128]{1,0:T(8,128)(2,1)S(1)}, s16[272,128]{1,0:T(8,128)(2,1)S(1)}, u32[]{:S(2)}, u32[]{:S(2)}) collective-permute-start(s16[272,128]{1,0:T(8,128)(2,1)S(1)} %level_states_0.1.refs_3_), channel_id=1, source_target_pairs={{0,8},{8,16},{16,24},{1,9},{9,17},{17,25},{2,10},{10,18},{18,26},{... | collective-permute-start | bytes 208904 | tf_op jit(solution)/shard_map/ppermute | solution.py:447
  24.3 4.5 %collective-permute-start.14 = (s16[272,128]{1,0:T(8,128)(2,1)S(1)}, s16[272,128]{1,0:T(8,128)(2,1)S(1)}, u32[]{:S(2)}, u32[]{:S(2)}) collective-permute-start(s16[272,128]{1,0:T(8,128)(2,1)S(1)} %level_states_0.1.refs_3_), channel_id=1, source_target_pairs={{0,16},{8,24},{1,17},{9,25},{2,18},{10,26},{3,19},{11,27},{4,20},{... | collective-permute-start | bytes 208904 | tf_op jit(solution)/shard_map/ppermute | solution.py:447
  28.8 0.0 collective-permute-done.4.refs_0_.refs_8_
  28.8 1.3 %collective-permute-start.13 = (s16[272,128]{1,0:T(8,128)(2,1)S(1)}, s16[272,128]{1,0:T(8,128)(2,1)S(1)}, u32[]{:S(2)}, u32[]{:S(2)}) collective-permute-start(s16[272,128]{1,0:T(8,128)(2,1)S(1)} %level_states_0.1.refs_3_), channel_id=1, source_target_pairs={{0,24},{1,25},{2,26},{3,27},{4,28},{5,29},{6,30},{7,31}} | collective-permute-start | bytes 208904 | tf_op jit(solution)/shard_map/ppermute | solution.py:447
  30.1 0.0 collective-permute-done.5.refs_1_.refs_9_
  30.1 1.5 %collective-permute-start.3 = (f32[1,1024]{1,0:T(1,128)S(1)}, f32[1,1024]{1,0:T(1,128)S(1)}, u32[]{:S(2)}, u32[]{:S(2)}) collective-permute-start(f32[1,1024]{1,0:T(1,128)S(1)} %bitcast.5), channel_id=1, source_target_pairs={{0,2},{2,0},{1,3},{3,1},{4,6},{6,4},{5,7},{7,5},{8,10},{10,8},{9,1... | collective-permute-start | bytes 12296 | tf_op jit(solution)/shard_map/ppermute | solution.py:440
  31.6 0.0 collective-permute-done.6.refs_2_.refs_10_
  31.6 0.1 level_states_1.1.refs_6_
  31.8 1.3 %collective-permute-start.12 = (s16[272,128]{1,0:T(8,128)(2,1)S(1)}, s16[272,128]{1,0:T(8,128)(2,1)S(1)}, u32[]{:S(2)}, u32[]{:S(2)}) collective-permute-start(s16[272,128]{1,0:T(8,128)(2,1)S(1)} %level_states_1.1.refs_6_), channel_id=1, source_target_pairs={{0,8},{8,16},{16,24},{1,9},{9,17},{17,25},{2,10},{10,18},{18,26},{... | collective-permute-start | bytes 208904 | tf_op jit(solution)/shard_map/ppermute | solution.py:447
  33.1 0.8 %collective-permute-done.3.refs_7_.gain_ref = f32[1,1024]{1,0:T(1,128)S(1)} collective-permute-done((f32[1,1024]{1,0:T(1,128)S(1)}, f32[1,1024]{1,0:T(1,128)S(1)}, u32[]{:S(2)}, u32[]{:S(2)}) %collective-permute-start.3) | collective-permute-done | bytes 4128 | tf_op jit(solution)/shard_map/ppermute | solution.py:440
  33.8 1.3 %collective-permute-start.11 = (s16[272,128]{1,0:T(8,128)(2,1)S(1)}, s16[272,128]{1,0:T(8,128)(2,1)S(1)}, u32[]{:S(2)}, u32[]{:S(2)}) collective-permute-start(s16[272,128]{1,0:T(8,128)(2,1)S(1)} %level_states_1.1.refs_6_), channel_id=1, source_target_pairs={{0,16},{8,24},{1,17},{9,25},{2,18},{10,26},{3,19},{11,27},{4,20},{... | collective-permute-start | bytes 208904 | tf_op jit(solution)/shard_map/ppermute | solution.py:447
  35.1 0.0 collective-permute-done.15.refs_5_.refs_6_
  35.1 1.3 %collective-permute-start.10 = (s16[272,128]{1,0:T(8,128)(2,1)S(1)}, s16[272,128]{1,0:T(8,128)(2,1)S(1)}, u32[]{:S(2)}, u32[]{:S(2)}) collective-permute-start(s16[272,128]{1,0:T(8,128)(2,1)S(1)} %level_states_1.1.refs_6_), channel_id=1, source_target_pairs={{0,24},{1,25},{2,26},{3,27},{4,28},{5,29},{6,30},{7,31}} | collective-permute-start | bytes 208904 | tf_op jit(solution)/shard_map/ppermute | solution.py:447
  36.4 0.0 collective-permute-done.14.refs_4_.refs_5_
  36.4 0.0 collective-permute-done.13.refs_3_.refs_4_
  36.4 0.8 %carries_0.1 = (s16[272,128]{1,0:T(8,128)(2,1)S(1)}, s16[272,128]{1,0:T(8,128)(2,1)S(1)}) custom-call(s32[4]{0:T(128)S(1)} %pad_add_fusion.place_ref, f32[2,128,128]{2,1,0:T(8,128)S(1)} %get-tuple-element.36.refs_0_.own_ref, s16[272,128]{1,0:T(8,128)(2,1)S(1)} %collective-permute-done.7.refs_0_.refs_1_, ...), custom_call_target="tpu_custom_call" | custom-call | bytes 1245184 | tf_op jit(solution)/shard_map/carries_0/pallas_call | solution.py:273
  37.2 2.4 %collective-permute-start.19 = (s16[272,128]{1,0:T(8,128)(2,1)S(1)}, s16[272,128]{1,0:T(8,128)(2,1)S(1)}, u32[]{:S(2)}, u32[]{:S(2)}) collective-permute-start(s16[272,128]{1,0:T(8,128)(2,1)S(1)} %get-tuple-element.49), channel_id=1, source_target_pairs={{0,6},{2,4},{4,2},{6,0},{1,7},{3,5},{5,3},{7,1},{8,14},{10,12},{12... | collective-permute-start | bytes 208904 | tf_op jit(solution)/shard_map/ppermute | solution.py:440
  39.6 0.5 collective-permute-start.18
  40.1 0.0 collective-permute-done.12.refs_5_.refs_13_
  40.1 0.0 collective-permute-done.11.refs_4_.refs_12_
  40.1 0.0 collective-permute-done.10.refs_3_.refs_11_
  40.1 0.8 %carries_1.1 = (s16[272,128]{1,0:T(8,128)(2,1)S(1)}, s16[272,128]{1,0:T(8,128)(2,1)S(1)}) custom-call(s32[4]{0:T(128)S(1)} %pad_add_fusion.place_ref, f32[2,128,128]{2,1,0:T(8,128)S(1)} %get-tuple-element.38.refs_3_.own_ref.refs_7_, s16[272,128]{1,0:T(8,128)(2,1)S(1)} %collective-permute-done.4.refs_0_.refs_8_, ...), custom_call_target="tpu_custom_call" | custom-call | bytes 1245184 | tf_op jit(solution)/shard_map/carries_1/pallas_call | solution.py:273
  40.9 1.6 %collective-permute-start.17 = (s16[272,128]{1,0:T(8,128)(2,1)S(1)}, s16[272,128]{1,0:T(8,128)(2,1)S(1)}, u32[]{:S(2)}, u32[]{:S(2)}) collective-permute-start(s16[272,128]{1,0:T(8,128)(2,1)S(1)} %get-tuple-element.47), channel_id=1, source_target_pairs={{0,6},{2,4},{4,2},{6,0},{1,7},{3,5},{5,3},{7,1},{8,14},{10,12},{12... | collective-permute-start | bytes 208904 | tf_op jit(solution)/shard_map/ppermute | solution.py:440
  42.5 0.6 collective-permute-start.16
  43.1 0.0 collective-permute-done.19.refs_1_
  43.1 1.1 %collective-permute-done.18.refs_0_ = s16[272,128]{1,0:T(8,128)(2,1)S(1)} collective-permute-done((s16[272,128]{1,0:T(8,128)(2,1)S(1)}, s16[272,128]{1,0:T(8,128)(2,1)S(1)}, u32[]{:S(2)}, u32[]{:S(2)}) %collective-permute-start.18) | collective-permute-done | bytes 69664 | tf_op jit(solution)/shard_map/ppermute | solution.py:440
  44.1 1.9 %attend_0_1_3.1.refs_2_ = bf16[512,512]{1,0:T(8,128)(2,1)S(1)} custom-call(s32[4]{0:T(128)S(1)} %pad_add_fusion.place_ref, bf16[256,2048]{1,0:T(8,128)(2,1)S(1)} %get-tuple-element.30.refs_0_.q_ref, bf16[256,2048]{1,0:T(8,128)(2,1)S(1)} %collective-permute-done.refs_1_.refs_4_.q_sib_ref, bf16[256,2048]{1,0:T(8,128)(2,1)S(1)} %get-tuple-element.32.k_ref, ...), custom_call_target="tpu_custom_call" | custom-call | flops 402653184 | bytes 2097152 | tf_op jit(solution)/shard_map/attend_0_1_3/pallas_call | solution.py:365
  46.0 0.6 collective-permute-start.22
  46.6 0.0 collective-permute-done.17.refs_1_
  46.6 1.2 %collective-permute-done.16.refs_0_ = s16[272,128]{1,0:T(8,128)(2,1)S(1)} collective-permute-done((s16[272,128]{1,0:T(8,128)(2,1)S(1)}, s16[272,128]{1,0:T(8,128)(2,1)S(1)}, u32[]{:S(2)}, u32[]{:S(2)}) %collective-permute-start.16) | collective-permute-done | bytes 69664 | tf_op jit(solution)/shard_map/ppermute | solution.py:440
  47.8 1.9 %attend_1_1_3.1.refs_14_.refs_2_ = bf16[512,512]{1,0:T(8,128)(2,1)S(1)} custom-call(s32[4]{0:T(128)S(1)} %pad_add_fusion.place_ref, bf16[256,2048]{1,0:T(8,128)(2,1)S(1)} %get-tuple-element.30.refs_0_.q_ref, bf16[256,2048]{1,0:T(8,128)(2,1)S(1)} %collective-permute-done.refs_1_.refs_4_.q_sib_ref, bf16[256,2048]{1,0:T(8,128)(2,1)S(1)} %get-tuple-element.32.k_ref, ...), custom_call_target="tpu_custom_call" | custom-call | flops 402653184 | bytes 2097152 | tf_op jit(solution)/shard_map/attend_1_1_3/pallas_call | solution.py:365
  49.7 1.2 %collective-permute-start.20 = (bf16[512,512]{1,0:T(8,128)(2,1)S(1)}, bf16[512,512]{1,0:T(8,128)(2,1)S(1)}, u32[]{:S(2)}, u32[]{:S(2)}) collective-permute-start(bf16[512,512]{1,0:T(8,128)(2,1)S(1)} %attend_1_1_3.1.refs_14_.refs_2_), channel_id=1, source_target_pairs={{0,2},{2,0},{1,3},{3,1},{4,6},{6,4},{5,7},{7,5},{8,10},{10,8},{9,1... | collective-permute-start | bytes 1572872 | tf_op jit(solution)/shard_map/ppermute | solution.py:440
  50.8 1.1 %own_carries.1 = (s16[528,128]{1,0:T(8,128)(2,1)S(1)}, s16[528,128]{1,0:T(8,128)(2,1)S(1)}, f32[2,2,128,128]{3,2,1,0:T(8,128)S(1)}, f32[2,2,128,128]{3,2,1,0:T(8,128)S(1)}) custom-call(s32[4]{0:T(128)S(1)} %pad_add_fusion.place_ref, f32[2,128,128]{2,1,0:T(8,128)S(1)} %get-tuple-element.36.refs_0_.own_ref, ...), custom_call_target="tpu_custom_call" | custom-call | bytes 2621440 | tf_op jit(solution)/shard_map/own_carries/pallas_call | solution.py:307
  52.0 1.0 %collective-permute-start.23 = (f32[2,2,128,128]{3,2,1,0:T(8,128)S(1)}, f32[2,2,128,128]{3,2,1,0:T(8,128)S(1)}, u32[]{:S(2)}, u32[]{:S(2)}) collective-permute-start(f32[2,2,128,128]{3,2,1,0:T(8,128)S(1)} %get-tuple-element.53), channel_id=1, source_target_pairs={{0,4},{4,0},{1,5},{5,1},{2,6},{6,2},{3,7},{7,3},{8,12},{12,8},{9,1... | collective-permute-start | bytes 786440 | tf_op jit(solution)/shard_map/ppermute | solution.py:440
  53.0 1.1 %collective-permute-start.21 = (s16[528,128]{1,0:T(8,128)(2,1)S(1)}, s16[528,128]{1,0:T(8,128)(2,1)S(1)}, u32[]{:S(2)}, u32[]{:S(2)}) collective-permute-start(s16[528,128]{1,0:T(8,128)(2,1)S(1)} %get-tuple-element.51), channel_id=1, source_target_pairs={{0,4},{2,6},{4,0},{6,2},{1,5},{3,7},{5,1},{7,3},{8,12},{10,14},{12... | collective-permute-start | bytes 405512 | tf_op jit(solution)/shard_map/ppermute | solution.py:440
  54.1 5.8 %collective-permute-done.21.refs_1_ = s16[528,128]{1,0:T(8,128)(2,1)S(1)} collective-permute-done((s16[528,128]{1,0:T(8,128)(2,1)S(1)}, s16[528,128]{1,0:T(8,128)(2,1)S(1)}, u32[]{:S(2)}, u32[]{:S(2)}) %collective-permute-start.21) | collective-permute-done | bytes 135200 | tf_op jit(solution)/shard_map/ppermute | solution.py:440
  59.9 1.9 %attend_0_0_2.1.refs_2_.refs_0_ = bf16[512,512]{1,0:T(8,128)(2,1)S(1)} custom-call(s32[4]{0:T(128)S(1)} %pad_add_fusion.place_ref, bf16[256,2048]{1,0:T(8,128)(2,1)S(1)} %get-tuple-element.30.refs_0_.q_ref, bf16[256,2048]{1,0:T(8,128)(2,1)S(1)} %collective-permute-done.refs_1_.refs_4_.q_sib_ref, bf16[256,2048]{1,0:T(8,128)(2,1)S(1)} %get-tuple-element.32.k_ref, ...), custom_call_target="tpu_custom_call" | custom-call | flops 402653184 | bytes 2097152 | tf_op jit(solution)/shard_map/attend_0_0_2/pallas_call | solution.py:365
  61.7 1.9 %attend_1_0_2.1.refs_1_ = bf16[512,512]{1,0:T(8,128)(2,1)S(1)} custom-call(s32[4]{0:T(128)S(1)} %pad_add_fusion.place_ref, bf16[256,2048]{1,0:T(8,128)(2,1)S(1)} %get-tuple-element.30.refs_0_.q_ref, bf16[256,2048]{1,0:T(8,128)(2,1)S(1)} %collective-permute-done.refs_1_.refs_4_.q_sib_ref, bf16[256,2048]{1,0:T(8,128)(2,1)S(1)} %get-tuple-element.32.k_ref, ...), custom_call_target="tpu_custom_call" | custom-call | flops 402653184 | bytes 2097152 | tf_op jit(solution)/shard_map/attend_1_0_2/pallas_call | solution.py:365
  63.6 0.0 collective-permute-done.23.refs_1_
  63.6 1.4 %assemble_cache.1 = f32[1,8,128,128]{3,2,1,0:T(8,128)} custom-call(s32[4]{0:T(128)S(1)} %pad_add_fusion.place_ref, f32[2,2,128,128]{3,2,1,0:T(8,128)S(1)} %get-tuple-element.52.refs_0_, f32[2,2,128,128]{3,2,1,0:T(8,128)S(1)} %collective-permute-done.23.refs_1_), custom_call_target="tpu_custom_call" | custom-call | tf_op jit(solution)/shard_map/assemble_cache/pallas_call | solution.py:425
  65.0 1.7 %assemble.1.refs_1_ = bf16[1024,1024]{1,0:T(8,128)(2,1)} custom-call(s32[4]{0:T(128)S(1)} %pad_add_fusion.place_ref, bf16[512,512]{1,0:T(8,128)(2,1)S(1)} %attend_0_0_2.1.refs_2_.refs_0_, bf16[512,512]{1,0:T(8,128)(2,1)S(1)} %attend_1_0_2.1.refs_1_, bf16[512,512]{1,0:T(8,128)(2,1)S(1)} %collective-permute-done.22.refs_2_), custom_call_target="tpu_custom_call" | custom-call | tf_op jit(solution)/shard_map/assemble/pallas_call | solution.py:404
  66.7 1.2 %collective-permute-done.20.refs_0_ = bf16[512,512]{1,0:T(8,128)(2,1)S(1)} collective-permute-done((bf16[512,512]{1,0:T(8,128)(2,1)S(1)}, bf16[512,512]{1,0:T(8,128)(2,1)S(1)}, u32[]{:S(2)}, u32[]{:S(2)}) %collective-permute-start.20) | collective-permute-done | bytes 524320 | tf_op jit(solution)/shard_map/ppermute | solution.py:440
  67.9 1.4 %finish.1 = bf16[1024,1024]{1,0:T(8,128)(2,1)} custom-call(s32[4]{0:T(128)S(1)} %pad_add_fusion.place_ref, bf16[512,512]{1,0:T(8,128)(2,1)S(1)} %collective-permute-done.20.refs_0_, bf16[1024,1024]{1,0:T(8,128)(2,1)} %assemble.1.refs_1_), custom_call_target="tpu_custom_call", output_to_operand_aliasing={{}: (2, {})} | custom-call | tf_op jit(solution)/shard_map/finish/pallas_call | solution.py:404
  (5 shorter events, 0.0 us)
Async XLA Ops:
  0.7 5.0 %copy-start = (bf16[256,4096]{1,0:T(8,128)(2,1)S(1)}, bf16[256,4096]{1,0:T(8,128)(2,1)}, u32[]{:S(2)}) copy-start(bf16[256,4096]{1,0:T(8,128)(2,1)} %queries_ref.1) | copy-start | bytes 6291460
  5.1 2.8 %collective-permute-start.1 = (bf16[256,2048]{1,0:T(8,128)(2,1)S(1)}, bf16[256,2048]{1,0:T(8,128)(2,1)S(1)}, u32[]{:S(2)}, u32[]{:S(2)}) collective-permute-start(bf16[256,2048]{1,0:T(8,128)(2,1)S(1)} %get-tuple-element.33), channel_id=1, source_target_pairs={{0,1},{1,0},{2,3},{3,2},{4,5},{5,4},{6,7},{7,6},{8,9},{9,8},{10,11... | collective-permute-start | bytes 3145736 | tf_op jit(solution)/shard_map/ppermute | solution.py:440
  5.6 3.8 %collective-permute-start.2 = (bf16[256,2048]{1,0:T(8,128)(2,1)S(1)}, bf16[256,2048]{1,0:T(8,128)(2,1)S(1)}, u32[]{:S(2)}, u32[]{:S(2)}) collective-permute-start(bf16[256,2048]{1,0:T(8,128)(2,1)S(1)} %get-tuple-element.35), channel_id=1, source_target_pairs={{0,1},{1,0},{2,3},{3,2},{4,5},{5,4},{6,7},{7,6},{8,9},{9,8},{10,11... | collective-permute-start | bytes 3145736 | tf_op jit(solution)/shard_map/ppermute | solution.py:440
  6.4 8.8 %collective-permute-start = (bf16[256,2048]{1,0:T(8,128)(2,1)S(1)}, bf16[256,2048]{1,0:T(8,128)(2,1)S(1)}, u32[]{:S(2)}, u32[]{:S(2)}) collective-permute-start(bf16[256,2048]{1,0:T(8,128)(2,1)S(1)} %get-tuple-element.31), channel_id=1, source_target_pairs={{0,1},{1,0},{2,3},{3,2},{4,5},{5,4},{6,7},{7,6},{8,9},{9,8},{10,11... | collective-permute-start | bytes 3145736 | tf_op jit(solution)/shard_map/ppermute | solution.py:440
  10.8 9.4 %collective-permute-start.7 = (s16[272,128]{1,0:T(8,128)(2,1)S(1)}, s16[272,128]{1,0:T(8,128)(2,1)S(1)}, u32[]{:S(2)}, u32[]{:S(2)}) collective-permute-start(s16[272,128]{1,0:T(8,128)(2,1)S(1)} %get-tuple-element.42), channel_id=1, source_target_pairs={{0,2},{2,0},{4,6},{6,4},{1,3},{3,1},{5,7},{7,5},{8,10},{10,8},{12,... | collective-permute-start | bytes 208904 | tf_op jit(solution)/shard_map/ppermute | solution.py:440
  13.7 6.5 %collective-permute-start.8 = (s16[272,128]{1,0:T(8,128)(2,1)S(1)}, s16[272,128]{1,0:T(8,128)(2,1)S(1)}, u32[]{:S(2)}, u32[]{:S(2)}) collective-permute-start(s16[272,128]{1,0:T(8,128)(2,1)S(1)} %get-tuple-element.43), channel_id=1, source_target_pairs={{0,4},{2,6},{4,0},{6,2},{1,5},{3,7},{5,1},{7,3},{8,12},{10,14},{12... | collective-permute-start | bytes 208904 | tf_op jit(solution)/shard_map/ppermute | solution.py:440
  15.2 5.7 %collective-permute-start.9 = (s16[272,128]{1,0:T(8,128)(2,1)S(1)}, s16[272,128]{1,0:T(8,128)(2,1)S(1)}, u32[]{:S(2)}, u32[]{:S(2)}) collective-permute-start(s16[272,128]{1,0:T(8,128)(2,1)S(1)} %get-tuple-element.44), channel_id=1, source_target_pairs={{0,6},{2,4},{4,2},{6,0},{1,7},{3,5},{5,3},{7,1},{8,14},{10,12},{12... | collective-permute-start | bytes 208904 | tf_op jit(solution)/shard_map/ppermute | solution.py:440
  15.3 14.9 %copy-start.1 = (f32[1024]{0:T(1024)S(1)}, f32[1024]{0:T(1024)}, u32[]{:S(2)}) copy-start(f32[1024]{0:T(1024)} %param.9) | copy-start | bytes 12292
  16.6 12.2 %collective-permute-start.4 = (s16[272,128]{1,0:T(8,128)(2,1)S(1)}, s16[272,128]{1,0:T(8,128)(2,1)S(1)}, u32[]{:S(2)}, u32[]{:S(2)}) collective-permute-start(s16[272,128]{1,0:T(8,128)(2,1)S(1)} %get-tuple-element.39), channel_id=1, source_target_pairs={{0,2},{2,0},{4,6},{6,4},{1,3},{3,1},{5,7},{7,5},{8,10},{10,8},{12,... | collective-permute-start | bytes 208904 | tf_op jit(solution)/shard_map/ppermute | solution.py:440
  18.6 11.5 %collective-permute-start.5 = (s16[272,128]{1,0:T(8,128)(2,1)S(1)}, s16[272,128]{1,0:T(8,128)(2,1)S(1)}, u32[]{:S(2)}, u32[]{:S(2)}) collective-permute-start(s16[272,128]{1,0:T(8,128)(2,1)S(1)} %get-tuple-element.40), channel_id=1, source_target_pairs={{0,4},{2,6},{4,0},{6,2},{1,5},{3,7},{5,1},{7,3},{8,12},{10,14},{12... | collective-permute-start | bytes 208904 | tf_op jit(solution)/shard_map/ppermute | solution.py:440
  20.1 11.5 %collective-permute-start.6 = (s16[272,128]{1,0:T(8,128)(2,1)S(1)}, s16[272,128]{1,0:T(8,128)(2,1)S(1)}, u32[]{:S(2)}, u32[]{:S(2)}) collective-permute-start(s16[272,128]{1,0:T(8,128)(2,1)S(1)} %get-tuple-element.41), channel_id=1, source_target_pairs={{0,6},{2,4},{4,2},{6,0},{1,7},{3,5},{5,3},{7,1},{8,14},{10,12},{12... | collective-permute-start | bytes 208904 | tf_op jit(solution)/shard_map/ppermute | solution.py:440
  21.0 14.1 %collective-permute-start.15 = (s16[272,128]{1,0:T(8,128)(2,1)S(1)}, s16[272,128]{1,0:T(8,128)(2,1)S(1)}, u32[]{:S(2)}, u32[]{:S(2)}) collective-permute-start(s16[272,128]{1,0:T(8,128)(2,1)S(1)} %level_states_0.1.refs_3_), channel_id=1, source_target_pairs={{0,8},{8,16},{16,24},{1,9},{9,17},{17,25},{2,10},{10,18},{18,26},{... | collective-permute-start | bytes 208904 | tf_op jit(solution)/shard_map/ppermute | solution.py:447
  24.3 12.1 %collective-permute-start.14 = (s16[272,128]{1,0:T(8,128)(2,1)S(1)}, s16[272,128]{1,0:T(8,128)(2,1)S(1)}, u32[]{:S(2)}, u32[]{:S(2)}) collective-permute-start(s16[272,128]{1,0:T(8,128)(2,1)S(1)} %level_states_0.1.refs_3_), channel_id=1, source_target_pairs={{0,16},{8,24},{1,17},{9,25},{2,18},{10,26},{3,19},{11,27},{4,20},{... | collective-permute-start | bytes 208904 | tf_op jit(solution)/shard_map/ppermute | solution.py:447
  28.8 7.6 %collective-permute-start.13 = (s16[272,128]{1,0:T(8,128)(2,1)S(1)}, s16[272,128]{1,0:T(8,128)(2,1)S(1)}, u32[]{:S(2)}, u32[]{:S(2)}) collective-permute-start(s16[272,128]{1,0:T(8,128)(2,1)S(1)} %level_states_0.1.refs_3_), channel_id=1, source_target_pairs={{0,24},{1,25},{2,26},{3,27},{4,28},{5,29},{6,30},{7,31}} | collective-permute-start | bytes 208904 | tf_op jit(solution)/shard_map/ppermute | solution.py:447
  30.1 3.7 %collective-permute-start.3 = (f32[1,1024]{1,0:T(1,128)S(1)}, f32[1,1024]{1,0:T(1,128)S(1)}, u32[]{:S(2)}, u32[]{:S(2)}) collective-permute-start(f32[1,1024]{1,0:T(1,128)S(1)} %bitcast.5), channel_id=1, source_target_pairs={{0,2},{2,0},{1,3},{3,1},{4,6},{6,4},{5,7},{7,5},{8,10},{10,8},{9,1... | collective-permute-start | bytes 12296 | tf_op jit(solution)/shard_map/ppermute | solution.py:440
  31.8 8.4 %collective-permute-start.12 = (s16[272,128]{1,0:T(8,128)(2,1)S(1)}, s16[272,128]{1,0:T(8,128)(2,1)S(1)}, u32[]{:S(2)}, u32[]{:S(2)}) collective-permute-start(s16[272,128]{1,0:T(8,128)(2,1)S(1)} %level_states_1.1.refs_6_), channel_id=1, source_target_pairs={{0,8},{8,16},{16,24},{1,9},{9,17},{17,25},{2,10},{10,18},{18,26},{... | collective-permute-start | bytes 208904 | tf_op jit(solution)/shard_map/ppermute | solution.py:447
  33.8 6.3 %collective-permute-start.11 = (s16[272,128]{1,0:T(8,128)(2,1)S(1)}, s16[272,128]{1,0:T(8,128)(2,1)S(1)}, u32[]{:S(2)}, u32[]{:S(2)}) collective-permute-start(s16[272,128]{1,0:T(8,128)(2,1)S(1)} %level_states_1.1.refs_6_), channel_id=1, source_target_pairs={{0,16},{8,24},{1,17},{9,25},{2,18},{10,26},{3,19},{11,27},{4,20},{... | collective-permute-start | bytes 208904 | tf_op jit(solution)/shard_map/ppermute | solution.py:447
  35.1 5.0 %collective-permute-start.10 = (s16[272,128]{1,0:T(8,128)(2,1)S(1)}, s16[272,128]{1,0:T(8,128)(2,1)S(1)}, u32[]{:S(2)}, u32[]{:S(2)}) collective-permute-start(s16[272,128]{1,0:T(8,128)(2,1)S(1)} %level_states_1.1.refs_6_), channel_id=1, source_target_pairs={{0,24},{1,25},{2,26},{3,27},{4,28},{5,29},{6,30},{7,31}} | collective-permute-start | bytes 208904 | tf_op jit(solution)/shard_map/ppermute | solution.py:447
  37.2 5.9 %collective-permute-start.19 = (s16[272,128]{1,0:T(8,128)(2,1)S(1)}, s16[272,128]{1,0:T(8,128)(2,1)S(1)}, u32[]{:S(2)}, u32[]{:S(2)}) collective-permute-start(s16[272,128]{1,0:T(8,128)(2,1)S(1)} %get-tuple-element.49), channel_id=1, source_target_pairs={{0,6},{2,4},{4,2},{6,0},{1,7},{3,5},{5,3},{7,1},{8,14},{10,12},{12... | collective-permute-start | bytes 208904 | tf_op jit(solution)/shard_map/ppermute | solution.py:440
  39.6 4.5 %collective-permute-start.18 = (s16[272,128]{1,0:T(8,128)(2,1)S(1)}, s16[272,128]{1,0:T(8,128)(2,1)S(1)}, u32[]{:S(2)}, u32[]{:S(2)}) collective-permute-start(s16[272,128]{1,0:T(8,128)(2,1)S(1)} %get-tuple-element.45.refs_6_), channel_id=1, source_target_pairs={{0,2},{2,0},{4,6},{6,4},{1,3},{3,1},{5,7},{7,5},{8,10},{10,8},{12,... | collective-permute-start | bytes 208904 | tf_op jit(solution)/shard_map/ppermute | solution.py:440
  40.9 5.7 %collective-permute-start.17 = (s16[272,128]{1,0:T(8,128)(2,1)S(1)}, s16[272,128]{1,0:T(8,128)(2,1)S(1)}, u32[]{:S(2)}, u32[]{:S(2)}) collective-permute-start(s16[272,128]{1,0:T(8,128)(2,1)S(1)} %get-tuple-element.47), channel_id=1, source_target_pairs={{0,6},{2,4},{4,2},{6,0},{1,7},{3,5},{5,3},{7,1},{8,14},{10,12},{12... | collective-permute-start | bytes 208904 | tf_op jit(solution)/shard_map/ppermute | solution.py:440
  42.5 5.4 %collective-permute-start.16 = (s16[272,128]{1,0:T(8,128)(2,1)S(1)}, s16[272,128]{1,0:T(8,128)(2,1)S(1)}, u32[]{:S(2)}, u32[]{:S(2)}) collective-permute-start(s16[272,128]{1,0:T(8,128)(2,1)S(1)} %get-tuple-element.46.refs_2_), channel_id=1, source_target_pairs={{0,2},{2,0},{4,6},{6,4},{1,3},{3,1},{5,7},{7,5},{8,10},{10,8},{12,... | collective-permute-start | bytes 208904 | tf_op jit(solution)/shard_map/ppermute | solution.py:440
  46.0 19.0 %collective-permute-start.22 = (bf16[512,512]{1,0:T(8,128)(2,1)S(1)}, bf16[512,512]{1,0:T(8,128)(2,1)S(1)}, u32[]{:S(2)}, u32[]{:S(2)}) collective-permute-start(bf16[512,512]{1,0:T(8,128)(2,1)S(1)} %attend_0_1_3.1.refs_2_), channel_id=1, source_target_pairs={{0,2},{2,0},{1,3},{3,1},{4,6},{6,4},{5,7},{7,5},{8,10},{10,8},{9,1... | collective-permute-start | bytes 1572872 | tf_op jit(solution)/shard_map/ppermute | solution.py:440
  49.7 18.2 %collective-permute-start.20 = (bf16[512,512]{1,0:T(8,128)(2,1)S(1)}, bf16[512,512]{1,0:T(8,128)(2,1)S(1)}, u32[]{:S(2)}, u32[]{:S(2)}) collective-permute-start(bf16[512,512]{1,0:T(8,128)(2,1)S(1)} %attend_1_1_3.1.refs_14_.refs_2_), channel_id=1, source_target_pairs={{0,2},{2,0},{1,3},{3,1},{4,6},{6,4},{5,7},{7,5},{8,10},{10,8},{9,1... | collective-permute-start | bytes 1572872 | tf_op jit(solution)/shard_map/ppermute | solution.py:440
  52.0 11.6 %collective-permute-start.23 = (f32[2,2,128,128]{3,2,1,0:T(8,128)S(1)}, f32[2,2,128,128]{3,2,1,0:T(8,128)S(1)}, u32[]{:S(2)}, u32[]{:S(2)}) collective-permute-start(f32[2,2,128,128]{3,2,1,0:T(8,128)S(1)} %get-tuple-element.53), channel_id=1, source_target_pairs={{0,4},{4,0},{1,5},{5,1},{2,6},{6,2},{3,7},{7,3},{8,12},{12,8},{9,1... | collective-permute-start | bytes 786440 | tf_op jit(solution)/shard_map/ppermute | solution.py:440
  53.0 6.9 %collective-permute-start.21 = (s16[528,128]{1,0:T(8,128)(2,1)S(1)}, s16[528,128]{1,0:T(8,128)(2,1)S(1)}, u32[]{:S(2)}, u32[]{:S(2)}) collective-permute-start(s16[528,128]{1,0:T(8,128)(2,1)S(1)} %get-tuple-element.51), channel_id=1, source_target_pairs={{0,4},{2,6},{4,0},{6,2},{1,5},{3,7},{5,1},{7,3},{8,12},{10,14},{12... | collective-permute-start | bytes 405512 | tf_op jit(solution)/shard_map/ppermute | solution.py:440

commit v8 on v7

--- a/solution.py
+++ b/solution.py
@@ -227,17 +227,35 @@
 
 def level_states(plan, own, others, half, after):
     def kernel(own_ref, *refs):
-        code(total_of((own_ref, *refs[: len(others)]), plan.each), refs[-1])
-
-    return pl.pallas_call(
-        kernel,
-        out_shape=coded_shape(plan.each),
+        total = total_of((own_ref, *refs[: len(others)]), plan.each)
+        for i, state in enumerate(total):
+            refs[-2][i] = state
+        code(total, refs[-1])
+
+    return pl.pallas_call(
+        kernel,
+        out_shape=[states_shape(plan.each), coded_shape(plan.each)],
         in_specs=[VMEM] * plan.plane + [ANY] * len(after),
-        out_specs=VMEM,
+        out_specs=[VMEM] * 2,
         compiler_params=params(),
         cost_estimate=cost(0, plan.plane * plan.each * HD * HD * 2),
         name=f"level_states_{half}",
     )(own, *others, *after)
+
+
+def levels_so_far(plan, total, arrived, half, after):
+    def kernel(total_ref, *refs):
+        code(total_of((total_ref, *refs[: len(arrived)]), plan.each), refs[-1])
+
+    return pl.pallas_call(
+        kernel,
+        out_shape=coded_shape(plan.each),
+        in_specs=[VMEM] * (1 + len(arrived)) + [ANY] * len(after),
+        out_specs=VMEM,
+        compiler_params=params(),
+        cost_estimate=cost(0, 2 * plan.each * HD * HD * 2),
+        name=f"levels_so_far_{half}_{len(arrived)}",
+    )(total, *arrived, *after)
 
 
 def carried(plan, place_ref, own, others, levels, offsets):
@@ -316,63 +334,95 @@
     )(place, *[a for arrays in operands for a in arrays], *after)
 
 
-def attend(plan, place, query, key, value, carry, first, gain, half, offsets, after=()):
+def attend_local(plan, place, query, key, value, half, offsets, after):
     rows = plan.rows
 
-    def kernel(
-        place_ref, q_ref, q_sib_ref, k_ref, k_sib_ref, v_ref, v_sib_ref, first_ref, gain_ref, *refs
-    ):
+    def kernel(place_ref, q_ref, q_sib_ref, k_ref, k_sib_ref, v_ref, v_sib_ref, *refs):
+        for piece, offset in enumerate(offsets):
+            for i in range(plan.each):
+                at = owned_columns(plan, place_ref, offset, half, i)
+                out_at = slice(piece * plan.piece + i * HD, piece * plan.piece + (i + 1) * HD)
+                refs[-1][0, :, out_at] = local_part(q_ref, k_ref, v_ref, at)
+                refs[-1][1, :, out_at] = local_part(q_sib_ref, k_sib_ref, v_sib_ref, at)
+
+    heads = len(offsets) * plan.each
+    return pl.pallas_call(
+        kernel,
+        out_shape=jax.ShapeDtypeStruct((CORES, rows, heads * HD), jnp.float32),
+        in_specs=[SMEM] + [VMEM] * 6 + [ANY] * len(after),
+        out_specs=VMEM,
+        compiler_params=params(),
+        cost_estimate=cost(heads * 8 * rows * rows * HD, 16 * rows * heads * HD),
+        name=f"attend_local_{half}_" + "_".join(map(str, offsets)),
+    )(place, *query, *key, *value, *after)
+
+
+def local_part(q_ref, k_ref, v_ref, at):
+    rows = q_ref.shape[0]
+    causal = lax.broadcasted_iota(jnp.int32, (rows, rows), 0) >= lax.broadcasted_iota(
+        jnp.int32, (rows, rows), 1
+    )
+    scores = contract_columns(q_ref[:, at], k_ref[:, at]) * SCORE_SCALE
+    weights = jnp.where(causal, scores, 0.0).astype(jnp.bfloat16)
+    return jnp.dot(weights, v_ref[:, at], preferred_element_type=jnp.float32)
+
+
+def finished(queries, local, carried, gain):
+    carried = carried * SCORE_SCALE
+    high = carried.astype(jnp.bfloat16)
+    low = (carried - high.astype(jnp.float32)).astype(jnp.bfloat16)
+    both = contract_columns(queries, jnp.concatenate([high, low], axis=0))
+    raw = local + (both[:, :HD] + both[:, HD:])
+    mean = jnp.mean(raw * raw, axis=-1, keepdims=True)
+    return (raw * lax.rsqrt(mean + 1e-06) * gain).astype(jnp.bfloat16)
+
+
+def attend(
+    plan, place, query, key, value, carry, first, gain, half, offsets, after=(), local=None
+):
+    rows = plan.rows
+    operands = [*query, local] if local is not None else [*query, *key, *value]
+    n = len(operands)
+
+    def kernel(place_ref, *refs):
         core = place_ref[0]
+        first_ref, gain_ref, *carry_refs = refs[n : n + 2 + len(offsets)]
         out_ref = refs[-1]
-        causal = lax.broadcasted_iota(jnp.int32, (rows, rows), 0) >= lax.broadcasted_iota(
-            jnp.int32, (rows, rows), 1
-        )
         is_second = jnp.full((HD, HD), core, jnp.int32) == 1
-
-        def attended(q_ref, k_ref, v_ref, at, carried, gain):
-            queries = q_ref[:, at]
-            scores = contract_columns(queries, k_ref[:, at]) * SCORE_SCALE
-            weights = jnp.where(causal, scores, 0.0).astype(jnp.bfloat16)
-            raw = jnp.dot(weights, v_ref[:, at], preferred_element_type=jnp.float32)
-            carried = carried * SCORE_SCALE
-            high = carried.astype(jnp.bfloat16)
-            low = (carried - high.astype(jnp.float32)).astype(jnp.bfloat16)
-            both = contract_columns(queries, jnp.concatenate([high, low], axis=0))
-            raw = raw + (both[:, :HD] + both[:, HD:])
-            mean = jnp.mean(raw * raw, axis=-1, keepdims=True)
-            return (raw * lax.rsqrt(mean + 1e-06) * gain).astype(jnp.bfloat16)
-
         for piece, offset in enumerate(offsets):
             x = place_ref[1] ^ (offset // plan.n_y)
-            carry_states = decoded(refs[piece])
+            carry_states = decoded(carry_refs[piece])
             skip = half * plan.each if len(carry_states) > plan.each else 0
             for i in range(plan.each):
                 at = owned_columns(plan, place_ref, offset, half, i)
                 start = ((half * plan.n_inner + x) * plan.each + i) * HD
                 gain = gain_ref[:, pl.ds(pl.multiple_of(start, HD), HD)]
                 out_at = slice(piece * plan.piece + i * HD, piece * plan.piece + (i + 1) * HD)
+                carried = carry_states[skip + i]
                 first = first_ref[offset, i]
-                mine = carry_states[skip + i] + jnp.where(is_second, first, 0.0)
-                sib = carry_states[skip + i] + jnp.where(is_second, 0.0, first)
-                out_ref[pl.ds(pl.multiple_of(core * rows, rows), rows), out_at] = attended(
-                    q_ref, k_ref, v_ref, at, mine, gain
-                )
-                out_ref[pl.ds(pl.multiple_of((1 - core) * rows, rows), rows), out_at] = attended(
-                    q_sib_ref, k_sib_ref, v_sib_ref, at, sib, gain
-                )
+                for side in range(CORES):
+                    if local is None:
+                        raw = local_part(refs[side], refs[2 + side], refs[4 + side], at)
+                    else:
+                        raw = refs[2][side, :, out_at]
+                    behind = is_second if side == 0 else ~is_second
+                    state = carried + jnp.where(behind, first, 0.0)
+                    of = core if side == 0 else 1 - core
+                    out_rows = pl.ds(pl.multiple_of(of * rows, rows), rows)
+                    out_ref[out_rows, out_at] = finished(refs[side][:, at], raw, state, gain)
 
     heads = len(offsets) * plan.each
     return pl.pallas_call(
         kernel,
         out_shape=jax.ShapeDtypeStruct((CORES * rows, heads * HD), jnp.bfloat16),
-        in_specs=[SMEM] + [VMEM] * (8 + len(offsets)) + [ANY] * len(after),
+        in_specs=[SMEM] + [VMEM] * (n + 2 + len(offsets)) + [ANY] * len(after),
         out_specs=VMEM,
         compiler_params=params(),
         cost_estimate=cost(
             heads * (8 * rows * rows * HD + 8 * rows * HD * HD), 16 * rows * heads * HD
         ),
         name=f"attend_{half}_" + "_".join(map(str, offsets)),
-    )(place, *query, *key, *value, first, gain, *carry, *after)
+    )(place, *operands, first, gain, *carry, *after)
 
 
 def assemble(plan, place, parts, into=None):
@@ -453,7 +503,7 @@
     query, query_out = spike_queries(plan, place, queries, counts)
     query = (query, swap(query_out, "core", 1, CORES))
 
-    own, first, others, levels, coded = [], [], [], [], []
+    own, first, others = [], [], []
 
     def owner_stage(half, after):
         mine, parts, *sends = chunk_states(plan, place, key, value, half, after)
@@ -461,15 +511,10 @@
         first.append(parts)
         others.append([in_level(a, o) for o, a in enumerate(sends, 1)])
 
-    def level_stage(half, after):
-        level = level_states(plan, own[half], others[half], half, after)
-        coded.append(level)
-        levels.append([to_later(level, d) for d in range(plan.n_outer - 1, 0, -1)])
-
     of_group = [list(range(y, plan.plane, plan.n_y)) for y in range(plan.n_y)]
     abroad = [o for offsets in of_group[1:] for o in offsets]
 
-    def part_of(half, offsets, carry, after):
+    def part_of(half, offsets, carry, after, local=None):
         return attend(
             plan,
             place,
@@ -482,6 +527,7 @@
             half,
             offsets,
             after,
+            local,
         )
 
     def carry_stage(half, after):
@@ -490,9 +536,9 @@
 
     parts = []
 
-    def send_stage(half, carry, after):
+    def send_stage(half, carry, after, local):
         for y in range(1, plan.n_y):
-            part = part_of(half, of_group[y], carry, after)
+            part = part_of(half, of_group[y], carry, after, local.get(y))
             parts.append((swap(part, "y", y, plan.n_y), half, of_group[y]))
             after = [part]
         return after
@@ -501,17 +547,33 @@
     for half in halves:
         owner_stage(half, after)
         after = [own[-1], query[1]]
+    totals, sums = [], []
     for half in halves:
-        level_stage(half, after)
-        after = [coded[-1]]
+        total, coded = level_states(plan, own[half], others[half], half, after)
+        totals.append(total)
+        sums.append(coded)
+        after = [coded]
+    levels = [[] for _ in halves]
+    distance = 1
+    after = [*after, *gains[1:]]
+    while distance < plan.n_outer:
+        for half in halves:
+            if distance > 1:
+                sums[half] = levels_so_far(plan, totals[half], levels[half], half, after)
+                after = [sums[half]]
+            levels[half].append(to_later(sums[half], distance))
+        distance *= 2
+    local = {}
+    for y in range(1, plan.n_y):
+        local[y] = attend_local(plan, place, query, key, value, 0, of_group[y], after)
+        after = [local[y]]
     carry = []
-    after = [*after, *gains[1:]]
     for half in halves:
         done, of_half = carry_stage(half, after)
         carry.append(of_half)
         after = [done]
     for half in halves:
-        after = send_stage(half, carry[half], after)
+        after = send_stage(half, carry[half], after, {} if half else local)
     sends = own_carries(plan, place, own, others, levels, of_group[0], after)
     own_carry = {o: in_level(a, o) if o else a for o, a in zip(of_group[0], sends)}
     caches = [

time: 69.5 us -> 72.2 us (1.039)
  waiting for transfers between devices: 13.2 us -> 15.9 us
  Pallas kernels: 22.6 us -> 23.4 us
    ppermute x18, waiting for transfers between devices: 13.2 us -> 15.9 us  [swap(): return lax.ppermute(array, axes, [(i, i ^ offset) for i in range(size)])]
    pallas_call x2 -> x5, Pallas kernels: 0.2 us -> 1.81 us  [the longest x1 1.48 us: attend_local(): pl.pallas_call(kernel, out_shape=jax.ShapeDtypeStruct((CORES, rows, heads...]
    pallas_call x4, Pallas kernels: 7.47 us -> 6.75 us  [attend(): pl.pallas_call(kernel, out_shape=jax.ShapeDtypeStruct((CORES * rows, head...]
    ppermute x6 -> x4, starting transfers between devices: 13 us -> 12.6 us  [to_later(): return lax.ppermute(array, 'outer', pairs)]
  transfers between devices with their start and end apart: 24 -> 22, of which waited for: 8 -> 9; matrix products, arithmetic and copies ran while one was open for 0% -> 0% of each run, Pallas kernels for 24% -> 25%
where the time goes in v8:
time: 72.2 us; the launch traced here: 72 us
  starting transfers between devices  31.8 us (44%)
  Pallas kernels  23.4 us (32%)
  waiting for transfers between devices  15.9 us (22%)
  between operations  0.85 us (1%)
    ppermute x18, starting transfers between devices, swap(): return lax.ppermute(array, axes, [(i, i ^ offset) for i in range(size)])  19.2 us
    ppermute x18, waiting for transfers between devices, swap(): return lax.ppermute(array, axes, [(i, i ^ offset) for i in range(size)])  15.9 us
    ppermute x4, starting transfers between devices, to_later(): return lax.ppermute(array, 'outer', pairs)  12.6 us
    pallas_call x4, Pallas kernels, attend(): pl.pallas_call(kernel, out_shape=jax.ShapeDtypeStruct((CORES * rows, head...  6.75 us
    pallas_call x1, Pallas kernels, decode(): pl.pallas_call(kernel, out_shape=[jax.ShapeDtypeStruct((rows, plan.n_y *...  4.36 us
    pallas_call x2, Pallas kernels, assemble(): pl.pallas_call(kernel, out_shape=jax.ShapeDtypeStruct((plan.n_y * rows, p...  3.08 us
    pallas_call x2, Pallas kernels, chunk_states(): pl.pallas_call(kernel, out_shape=[states_shape(plan.each), states_shape(p...  2.73 us
    pallas_call x1, Pallas kernels, attend_local(): pl.pallas_call(kernel, out_shape=jax.ShapeDtypeStruct((CORES, rows, heads...  1.48 us
  transfers between devices with their start and end apart: 22, of which 9 were waited for; matrix products, arithmetic and copies ran while one was open for 0% of the time, Pallas kernels for 25%

profile of v8, /device:TPU:0, one launch (start us, length us, event | category | flops | bytes accessed | tf_op | source)
XLA Modules:
  0.0 72.0 jit_solution(4192860738004652533)
XLA Ops:
  0.6 0.1 pad_add_fusion.place_ref
  0.7 4.4 %decode.1 = (bf16[256,2048]{1,0:T(8,128)(2,1)S(1)}, bf16[256,2048]{1,0:T(8,128)(2,1)S(1)}, bf16[256,2048]{1,0:T(8,128)(2,1)S(1)}, bf16[256,2048]{1,0:T(8,128)(2,...) custom-call(s32[4]{0:T(128)S(1)} %pad_add_fusion.place_ref, s32[256,4096]{1,0:T(8,128)} %refs_0_.1, ...), custom_call_target="tpu_custom_call" | custom-call | flops 4194304 | bytes 14680064 | tf_op jit(solution)/shard_map/decode/pallas_call | solution.py:100
  5.1 0.5 collective-permute-start.1
  5.6 0.1 collective-permute-start.2
  5.7 0.8 %spike_queries.1 = (bf16[256,2048]{1,0:T(8,128)(2,1)S(1)}, bf16[256,2048]{1,0:T(8,128)(2,1)S(1)}) custom-call(s32[4]{0:T(128)S(1)} %pad_add_fusion.place_ref, bf16[256,4096]{1,0:T(8,128)(2,1)S(1)} %copy-done, bf16[256,2048]{1,0:T(8,128)(2,1)S(1)} %get-tuple-element.32.refs_0_, bf16[256,2048]{1,0:T(8,128)(2,1)S(1)} %get-tuple-element.33.refs_1_), custom_call_target="tpu_custom_call" | custom-call | flops 1048576 | bytes 6291456 | tf_op jit(solution)/shard_map/spike_queries/pallas_call | solution.py:122
  6.4 0.5 collective-permute-start
  6.9 0.9 %collective-permute-done.1.k_sib_ref.refs_3_ = bf16[256,2048]{1,0:T(8,128)(2,1)S(1)} collective-permute-done((bf16[256,2048]{1,0:T(8,128)(2,1)S(1)}, bf16[256,2048]{1,0:T(8,128)(2,1)S(1)}, u32[]{:S(2)}, u32[]{:S(2)}) %collective-permute-start.1) | collective-permute-done | bytes 1048608 | tf_op jit(solution)/shard_map/ppermute | solution.py:490
  7.9 1.5 %collective-permute-done.2.v_sib_ref.refs_5_ = bf16[256,2048]{1,0:T(8,128)(2,1)S(1)} collective-permute-done((bf16[256,2048]{1,0:T(8,128)(2,1)S(1)}, bf16[256,2048]{1,0:T(8,128)(2,1)S(1)}, u32[]{:S(2)}, u32[]{:S(2)}) %collective-permute-start.2) | collective-permute-done | bytes 1048608 | tf_op jit(solution)/shard_map/ppermute | solution.py:490
  9.4 1.4 %chunk_states_0.1 = (f32[2,128,128]{2,1,0:T(8,128)S(1)}, f32[4,2,128,128]{3,2,1,0:T(8,128)S(1)}, s16[272,128]{1,0:T(8,128)(2,1)S(1)}, s16[272,128]{1,0:T(8,128)(2,1)S(1)}, s16[272,128]{1,0:T(8,128)(2,1)S(1)}) custom-call(s32[4]{0:T(128)S(1)} %pad_add_fusion.place_ref, bf16[256,2048]{1,0:T(8,128)(2,1)S(1)} %get-tuple-element.36.k_ref.refs_2_, ...), custom_call_target="tpu_custom_call" | custom-call | flops 134217728 | bytes 2883584 | tf_op jit(solution)/shard_map/chunk_states_0/pallas_call | solution.py:214
  10.8 3.0 %collective-permute-start.7 = (s16[272,128]{1,0:T(8,128)(2,1)S(1)}, s16[272,128]{1,0:T(8,128)(2,1)S(1)}, u32[]{:S(2)}, u32[]{:S(2)}) collective-permute-start(s16[272,128]{1,0:T(8,128)(2,1)S(1)} %get-tuple-element.46), channel_id=1, source_target_pairs={{0,2},{2,0},{4,6},{6,4},{1,3},{3,1},{5,7},{7,5},{8,10},{10,8},{12,... | collective-permute-start | bytes 208904 | tf_op jit(solution)/shard_map/ppermute | solution.py:490
  13.7 1.5 %collective-permute-start.8 = (s16[272,128]{1,0:T(8,128)(2,1)S(1)}, s16[272,128]{1,0:T(8,128)(2,1)S(1)}, u32[]{:S(2)}, u32[]{:S(2)}) collective-permute-start(s16[272,128]{1,0:T(8,128)(2,1)S(1)} %get-tuple-element.47), channel_id=1, source_target_pairs={{0,4},{2,6},{4,0},{6,2},{1,5},{3,7},{5,1},{7,3},{8,12},{10,14},{12... | collective-permute-start | bytes 208904 | tf_op jit(solution)/shard_map/ppermute | solution.py:490
  15.2 0.0 collective-permute-start.9
  15.3 0.0 collective-permute-done.refs_1_.refs_4_.q_sib_ref
  15.3 1.4 %chunk_states_1.1 = (f32[2,128,128]{2,1,0:T(8,128)S(1)}, f32[4,2,128,128]{3,2,1,0:T(8,128)S(1)}, s16[272,128]{1,0:T(8,128)(2,1)S(1)}, s16[272,128]{1,0:T(8,128)(2,1)S(1)}, s16[272,128]{1,0:T(8,128)(2,1)S(1)}) custom-call(s32[4]{0:T(128)S(1)} %pad_add_fusion.place_ref, bf16[256,2048]{1,0:T(8,128)(2,1)S(1)} %get-tuple-element.36.k_ref.refs_2_, ...), custom_call_target="tpu_custom_call" | custom-call | flops 134217728 | bytes 2883584 | tf_op jit(solution)/shard_map/chunk_states_1/pallas_call | solution.py:214
  16.6 2.0 %collective-permute-start.4 = (s16[272,128]{1,0:T(8,128)(2,1)S(1)}, s16[272,128]{1,0:T(8,128)(2,1)S(1)}, u32[]{:S(2)}, u32[]{:S(2)}) collective-permute-start(s16[272,128]{1,0:T(8,128)(2,1)S(1)} %get-tuple-element.43), channel_id=1, source_target_pairs={{0,2},{2,0},{4,6},{6,4},{1,3},{3,1},{5,7},{7,5},{8,10},{10,8},{12,... | collective-permute-start | bytes 208904 | tf_op jit(solution)/shard_map/ppermute | solution.py:490
  18.6 1.5 %collective-permute-start.5 = (s16[272,128]{1,0:T(8,128)(2,1)S(1)}, s16[272,128]{1,0:T(8,128)(2,1)S(1)}, u32[]{:S(2)}, u32[]{:S(2)}) collective-permute-start(s16[272,128]{1,0:T(8,128)(2,1)S(1)} %get-tuple-element.44), channel_id=1, source_target_pairs={{0,4},{2,6},{4,0},{6,2},{1,5},{3,7},{5,1},{7,3},{8,12},{10,14},{12... | collective-permute-start | bytes 208904 | tf_op jit(solution)/shard_map/ppermute | solution.py:490
  20.1 0.0 collective-permute-done.7.refs_0_.refs_1_
  20.1 0.0 collective-permute-start.6
  20.2 0.0 collective-permute-done.8.refs_1_.refs_2_
  20.2 0.7 collective-permute-done.9.refs_2_.refs_3_
  20.9 0.1 level_states_0.1
  21.0 3.3 %collective-permute-start.11 = (s16[272,128]{1,0:T(8,128)(2,1)S(1)}, s16[272,128]{1,0:T(8,128)(2,1)S(1)}, u32[]{:S(2)}, u32[]{:S(2)}) collective-permute-start(s16[272,128]{1,0:T(8,128)(2,1)S(1)} %get-tuple-element.49.refs_3_), channel_id=1, source_target_pairs={{0,8},{8,16},{16,24},{1,9},{9,17},{17,25},{2,10},{10,18},{18,26},{... | collective-permute-start | bytes 208904 | tf_op jit(solution)/shard_map/ppermute | solution.py:497
  24.3 0.0 collective-permute-done.4.refs_0_.refs_7_
  24.3 0.0 collective-permute-done.5.refs_1_.refs_8_
  24.3 1.0 %collective-permute-done.6.refs_2_.refs_9_ = s16[272,128]{1,0:T(8,128)(2,1)S(1)} collective-permute-done((s16[272,128]{1,0:T(8,128)(2,1)S(1)}, s16[272,128]{1,0:T(8,128)(2,1)S(1)}, u32[]{:S(2)}, u32[]{:S(2)}) %collective-permute-start.6) | collective-permute-done | bytes 69664 | tf_op jit(solution)/shard_map/ppermute | solution.py:490
  25.4 0.1 level_states_1.1
  25.5 3.5 %collective-permute-start.10 = (s16[272,128]{1,0:T(8,128)(2,1)S(1)}, s16[272,128]{1,0:T(8,128)(2,1)S(1)}, u32[]{:S(2)}, u32[]{:S(2)}) collective-permute-start(s16[272,128]{1,0:T(8,128)(2,1)S(1)} %get-tuple-element.50.refs_1_), channel_id=1, source_target_pairs={{0,8},{8,16},{16,24},{1,9},{9,17},{17,25},{2,10},{10,18},{18,26},{... | collective-permute-start | bytes 208904 | tf_op jit(solution)/shard_map/ppermute | solution.py:497
  29.0 0.6 collective-permute-start.3
  29.5 3.1 %collective-permute-done.3.refs_2_.refs_4_.refs_7_ = f32[1,1024]{1,0:T(1,128)S(1)} collective-permute-done((f32[1,1024]{1,0:T(1,128)S(1)}, f32[1,1024]{1,0:T(1,128)S(1)}, u32[]{:S(2)}, u32[]{:S(2)}) %collective-permute-start.3) | collective-permute-done | bytes 4128 | tf_op jit(solution)/shard_map/ppermute | solution.py:490
  32.6 0.0 collective-permute-done.11.refs_0_.refs_3_.refs_4_
  32.6 0.1 levels_so_far_0_1.1.refs_1_
  32.7 4.5 %collective-permute-start.13 = (s16[272,128]{1,0:T(8,128)(2,1)S(1)}, s16[272,128]{1,0:T(8,128)(2,1)S(1)}, u32[]{:S(2)}, u32[]{:S(2)}) collective-permute-start(s16[272,128]{1,0:T(8,128)(2,1)S(1)} %levels_so_far_0_1.1.refs_1_), channel_id=1, source_target_pairs={{0,16},{8,24},{1,17},{9,25},{2,18},{10,26},{3,19},{11,27},{4,20},{... | collective-permute-start | bytes 208904 | tf_op jit(solution)/shard_map/ppermute | solution.py:497
  37.2 0.0 collective-permute-done.10.refs_0_.refs_3_.refs_10_
  37.2 0.1 levels_so_far_1_1.1.refs_0_
  37.3 1.3 %collective-permute-start.12 = (s16[272,128]{1,0:T(8,128)(2,1)S(1)}, s16[272,128]{1,0:T(8,128)(2,1)S(1)}, u32[]{:S(2)}, u32[]{:S(2)}) collective-permute-start(s16[272,128]{1,0:T(8,128)(2,1)S(1)} %levels_so_far_1_1.1.refs_0_), channel_id=1, source_target_pairs={{0,16},{8,24},{1,17},{9,25},{2,18},{10,26},{3,19},{11,27},{4,20},{... | collective-permute-start | bytes 208904 | tf_op jit(solution)/shard_map/ppermute | solution.py:497
  38.6 1.5 %attend_local_0_1_3.1.refs_5_.refs_2_ = f32[2,256,512]{2,1,0:T(8,128)S(1)} custom-call(s32[4]{0:T(128)S(1)} %pad_add_fusion.place_ref, bf16[256,2048]{1,0:T(8,128)(2,1)S(1)} %get-tuple-element.34.refs_0_.q_ref, bf16[256,2048]{1,0:T(8,128)(2,1)S(1)} %collective-permute-done.refs_1_.refs_4_.q_sib_ref, bf16[256,2048]{1,0:T(8,128)(2,1)S(1)} %get-tuple-element.36.k_ref.refs_2_, ...), custom_call_target="tpu_custom_call" | custom-call | flops 268435456 | bytes 2097152 | tf_op jit(solution)/shard_map/attend_local_0_1_3/pallas_call | solution.py:349
  40.1 0.0 collective-permute-done.13.refs_4_.refs_5_
  40.1 0.7 %carries_0.1 = (s16[272,128]{1,0:T(8,128)(2,1)S(1)}, s16[272,128]{1,0:T(8,128)(2,1)S(1)}) custom-call(s32[4]{0:T(128)S(1)} %pad_add_fusion.place_ref, f32[2,128,128]{2,1,0:T(8,128)S(1)} %get-tuple-element.40.refs_0_.own_ref, s16[272,128]{1,0:T(8,128)(2,1)S(1)} %collective-permute-done.7.refs_0_.refs_1_, ...), custom_call_target="tpu_custom_call" | custom-call | bytes 1179648 | tf_op jit(solution)/shard_map/carries_0/pallas_call | solution.py:291
  40.8 0.8 %collective-permute-start.17 = (s16[272,128]{1,0:T(8,128)(2,1)S(1)}, s16[272,128]{1,0:T(8,128)(2,1)S(1)}, u32[]{:S(2)}, u32[]{:S(2)}) collective-permute-start(s16[272,128]{1,0:T(8,128)(2,1)S(1)} %get-tuple-element.57), channel_id=1, source_target_pairs={{0,6},{2,4},{4,2},{6,0},{1,7},{3,5},{5,3},{7,1},{8,14},{10,12},{12... | collective-permute-start | bytes 208904 | tf_op jit(solution)/shard_map/ppermute | solution.py:490
  41.6 1.3 %collective-permute-start.16 = (s16[272,128]{1,0:T(8,128)(2,1)S(1)}, s16[272,128]{1,0:T(8,128)(2,1)S(1)}, u32[]{:S(2)}, u32[]{:S(2)}) collective-permute-start(s16[272,128]{1,0:T(8,128)(2,1)S(1)} %get-tuple-element.53.refs_5_), channel_id=1, source_target_pairs={{0,2},{2,0},{4,6},{6,4},{1,3},{3,1},{5,7},{7,5},{8,10},{10,8},{12,... | collective-permute-start | bytes 208904 | tf_op jit(solution)/shard_map/ppermute | solution.py:490
  42.9 0.0 collective-permute-done.12.refs_4_.refs_11_
  42.9 0.7 %carries_1.1 = (s16[272,128]{1,0:T(8,128)(2,1)S(1)}, s16[272,128]{1,0:T(8,128)(2,1)S(1)}) custom-call(s32[4]{0:T(128)S(1)} %pad_add_fusion.place_ref, f32[2,128,128]{2,1,0:T(8,128)S(1)} %get-tuple-element.42.refs_3_.own_ref.refs_6_, s16[272,128]{1,0:T(8,128)(2,1)S(1)} %collective-permute-done.4.refs_0_.refs_7_, ...), custom_call_target="tpu_custom_call" | custom-call | bytes 1179648 | tf_op jit(solution)/shard_map/carries_1/pallas_call | solution.py:291
  43.6 1.5 %collective-permute-start.15 = (s16[272,128]{1,0:T(8,128)(2,1)S(1)}, s16[272,128]{1,0:T(8,128)(2,1)S(1)}, u32[]{:S(2)}, u32[]{:S(2)}) collective-permute-start(s16[272,128]{1,0:T(8,128)(2,1)S(1)} %get-tuple-element.55), channel_id=1, source_target_pairs={{0,6},{2,4},{4,2},{6,0},{1,7},{3,5},{5,3},{7,1},{8,14},{10,12},{12... | collective-permute-start | bytes 208904 | tf_op jit(solution)/shard_map/ppermute | solution.py:490
  45.1 1.5 %collective-permute-start.14 = (s16[272,128]{1,0:T(8,128)(2,1)S(1)}, s16[272,128]{1,0:T(8,128)(2,1)S(1)}, u32[]{:S(2)}, u32[]{:S(2)}) collective-permute-start(s16[272,128]{1,0:T(8,128)(2,1)S(1)} %get-tuple-element.54.refs_7_), channel_id=1, source_target_pairs={{0,2},{2,0},{4,6},{6,4},{1,3},{3,1},{5,7},{7,5},{8,10},{10,8},{12,... | collective-permute-start | bytes 208904 | tf_op jit(solution)/shard_map/ppermute | solution.py:490
  46.7 0.0 collective-permute-done.17.refs_6_
  46.7 0.5 collective-permute-done.16.refs_5_
  47.2 1.1 %attend_0_1_3.1.refs_10_ = bf16[512,512]{1,0:T(8,128)(2,1)S(1)} custom-call(s32[4]{0:T(128)S(1)} %pad_add_fusion.place_ref, bf16[256,2048]{1,0:T(8,128)(2,1)S(1)} %get-tuple-element.34.refs_0_.q_ref, bf16[256,2048]{1,0:T(8,128)(2,1)S(1)} %collective-permute-done.refs_1_.refs_4_.q_sib_ref, f32[2,256,512]{2,1,0:T(8,128)S(1)} %attend_local_0_1_3.1.refs_5_.refs_2_, ...), custom_call_target="tpu_custom_call" | custom-call | flops 402653184 | bytes 2097152 | tf_op jit(solution)/shard_map/attend_0_1_3/pallas_call | solution.py:415
  48.3 1.0 %collective-permute-start.20 = (bf16[512,512]{1,0:T(8,128)(2,1)S(1)}, bf16[512,512]{1,0:T(8,128)(2,1)S(1)}, u32[]{:S(2)}, u32[]{:S(2)}) collective-permute-start(bf16[512,512]{1,0:T(8,128)(2,1)S(1)} %attend_0_1_3.1.refs_10_), channel_id=1, source_target_pairs={{0,2},{2,0},{1,3},{3,1},{4,6},{6,4},{5,7},{7,5},{8,10},{10,8},{9,1... | collective-permute-start | bytes 1572872 | tf_op jit(solution)/shard_map/ppermute | solution.py:490
  49.3 0.0 collective-permute-done.15.refs_9_
  49.3 1.2 %collective-permute-done.14.refs_8_ = s16[272,128]{1,0:T(8,128)(2,1)S(1)} collective-permute-done((s16[272,128]{1,0:T(8,128)(2,1)S(1)}, s16[272,128]{1,0:T(8,128)(2,1)S(1)}, u32[]{:S(2)}, u32[]{:S(2)}) %collective-permute-start.14) | collective-permute-done | bytes 69664 | tf_op jit(solution)/shard_map/ppermute | solution.py:490
  50.6 1.9 %attend_1_1_3.1.refs_12_.refs_10_ = bf16[512,512]{1,0:T(8,128)(2,1)S(1)} custom-call(s32[4]{0:T(128)S(1)} %pad_add_fusion.place_ref, bf16[256,2048]{1,0:T(8,128)(2,1)S(1)} %get-tuple-element.34.refs_0_.q_ref, bf16[256,2048]{1,0:T(8,128)(2,1)S(1)} %collective-permute-done.refs_1_.refs_4_.q_sib_ref, bf16[256,2048]{1,0:T(8,128)(2,1)S(1)} %get-tuple-element.36.k_ref.refs_2_, ...), custom_call_target="tpu_custom_call" | custom-call | flops 402653184 | bytes 2097152 | tf_op jit(solution)/shard_map/attend_1_1_3/pallas_call | solution.py:415
  52.4 1.3 %collective-permute-start.18 = (bf16[512,512]{1,0:T(8,128)(2,1)S(1)}, bf16[512,512]{1,0:T(8,128)(2,1)S(1)}, u32[]{:S(2)}, u32[]{:S(2)}) collective-permute-start(bf16[512,512]{1,0:T(8,128)(2,1)S(1)} %attend_1_1_3.1.refs_12_.refs_10_), channel_id=1, source_target_pairs={{0,2},{2,0},{1,3},{3,1},{4,6},{6,4},{5,7},{7,5},{8,10},{10,8},{9,1... | collective-permute-start | bytes 1572872 | tf_op jit(solution)/shard_map/ppermute | solution.py:490
  53.7 1.1 %own_carries.1 = (s16[528,128]{1,0:T(8,128)(2,1)S(1)}, s16[528,128]{1,0:T(8,128)(2,1)S(1)}, f32[2,2,128,128]{3,2,1,0:T(8,128)S(1)}, f32[2,2,128,128]{3,2,1,0:T(8,128)S(1)}) custom-call(s32[4]{0:T(128)S(1)} %pad_add_fusion.place_ref, f32[2,128,128]{2,1,0:T(8,128)S(1)} %get-tuple-element.40.refs_0_.own_ref, ...), custom_call_target="tpu_custom_call" | custom-call | bytes 2621440 | tf_op jit(solution)/shard_map/own_carries/pallas_call | solution.py:325
  54.8 0.9 %collective-permute-start.21 = (f32[2,2,128,128]{3,2,1,0:T(8,128)S(1)}, f32[2,2,128,128]{3,2,1,0:T(8,128)S(1)}, u32[]{:S(2)}, u32[]{:S(2)}) collective-permute-start(f32[2,2,128,128]{3,2,1,0:T(8,128)S(1)} %get-tuple-element.61), channel_id=1, source_target_pairs={{0,4},{4,0},{1,5},{5,1},{2,6},{6,2},{3,7},{7,3},{8,12},{12,8},{9,1... | collective-permute-start | bytes 786440 | tf_op jit(solution)/shard_map/ppermute | solution.py:490
  55.6 1.2 %collective-permute-start.19 = (s16[528,128]{1,0:T(8,128)(2,1)S(1)}, s16[528,128]{1,0:T(8,128)(2,1)S(1)}, u32[]{:S(2)}, u32[]{:S(2)}) collective-permute-start(s16[528,128]{1,0:T(8,128)(2,1)S(1)} %get-tuple-element.59), channel_id=1, source_target_pairs={{0,4},{2,6},{4,0},{6,2},{1,5},{3,7},{5,1},{7,3},{8,12},{10,14},{12... | collective-permute-start | bytes 405512 | tf_op jit(solution)/shard_map/ppermute | solution.py:490
  56.9 5.8 %collective-permute-done.19.refs_9_ = s16[528,128]{1,0:T(8,128)(2,1)S(1)} collective-permute-done((s16[528,128]{1,0:T(8,128)(2,1)S(1)}, s16[528,128]{1,0:T(8,128)(2,1)S(1)}, u32[]{:S(2)}, u32[]{:S(2)}) %collective-permute-start.19) | collective-permute-done | bytes 135200 | tf_op jit(solution)/shard_map/ppermute | solution.py:490
  62.7 1.9 %attend_0_0_2.1.refs_10_.refs_0_ = bf16[512,512]{1,0:T(8,128)(2,1)S(1)} custom-call(s32[4]{0:T(128)S(1)} %pad_add_fusion.place_ref, bf16[256,2048]{1,0:T(8,128)(2,1)S(1)} %get-tuple-element.34.refs_0_.q_ref, bf16[256,2048]{1,0:T(8,128)(2,1)S(1)} %collective-permute-done.refs_1_.refs_4_.q_sib_ref, bf16[256,2048]{1,0:T(8,128)(2,1)S(1)} %get-tuple-element.36.k_ref.refs_2_, ...), custom_call_target="tpu_custom_call" | custom-call | flops 402653184 | bytes 2097152 | tf_op jit(solution)/shard_map/attend_0_0_2/pallas_call | solution.py:415
  64.5 1.9 %attend_1_0_2.1.refs_1_ = bf16[512,512]{1,0:T(8,128)(2,1)S(1)} custom-call(s32[4]{0:T(128)S(1)} %pad_add_fusion.place_ref, bf16[256,2048]{1,0:T(8,128)(2,1)S(1)} %get-tuple-element.34.refs_0_.q_ref, bf16[256,2048]{1,0:T(8,128)(2,1)S(1)} %collective-permute-done.refs_1_.refs_4_.q_sib_ref, bf16[256,2048]{1,0:T(8,128)(2,1)S(1)} %get-tuple-element.36.k_ref.refs_2_, ...), custom_call_target="tpu_custom_call" | custom-call | flops 402653184 | bytes 2097152 | tf_op jit(solution)/shard_map/attend_1_0_2/pallas_call | solution.py:415
  66.4 0.0 collective-permute-done.21.refs_1_
  66.4 1.4 %assemble_cache.1 = f32[1,8,128,128]{3,2,1,0:T(8,128)} custom-call(s32[4]{0:T(128)S(1)} %pad_add_fusion.place_ref, f32[2,2,128,128]{3,2,1,0:T(8,128)S(1)} %get-tuple-element.60.refs_0_, f32[2,2,128,128]{3,2,1,0:T(8,128)S(1)} %collective-permute-done.21.refs_1_), custom_call_target="tpu_custom_call" | custom-call | tf_op jit(solution)/shard_map/assemble_cache/pallas_call | solution.py:475
  67.8 0.0 collective-permute-done.20.refs_2_
  67.8 1.7 %assemble.1.refs_1_ = bf16[1024,1024]{1,0:T(8,128)(2,1)} custom-call(s32[4]{0:T(128)S(1)} %pad_add_fusion.place_ref, bf16[512,512]{1,0:T(8,128)(2,1)S(1)} %attend_0_0_2.1.refs_10_.refs_0_, bf16[512,512]{1,0:T(8,128)(2,1)S(1)} %attend_1_0_2.1.refs_1_, bf16[512,512]{1,0:T(8,128)(2,1)S(1)} %collective-permute-done.20.refs_2_), custom_call_target="tpu_custom_call" | custom-call | tf_op jit(solution)/shard_map/assemble/pallas_call | solution.py:454
  69.5 1.1 %collective-permute-done.18.refs_0_ = bf16[512,512]{1,0:T(8,128)(2,1)S(1)} collective-permute-done((bf16[512,512]{1,0:T(8,128)(2,1)S(1)}, bf16[512,512]{1,0:T(8,128)(2,1)S(1)}, u32[]{:S(2)}, u32[]{:S(2)}) %collective-permute-start.18) | collective-permute-done | bytes 524320 | tf_op jit(solution)/shard_map/ppermute | solution.py:490
  70.7 1.4 %finish.1 = bf16[1024,1024]{1,0:T(8,128)(2,1)} custom-call(s32[4]{0:T(128)S(1)} %pad_add_fusion.place_ref, bf16[512,512]{1,0:T(8,128)(2,1)S(1)} %collective-permute-done.18.refs_0_, bf16[1024,1024]{1,0:T(8,128)(2,1)} %assemble.1.refs_1_), custom_call_target="tpu_custom_call", output_to_operand_aliasing={{}: (2, {})} | custom-call | tf_op jit(solution)/shard_map/finish/pallas_call | solution.py:454
  (4 shorter events, 0.0 us)
Async XLA Ops:
  0.7 5.0 %copy-start = (bf16[256,4096]{1,0:T(8,128)(2,1)S(1)}, bf16[256,4096]{1,0:T(8,128)(2,1)}, u32[]{:S(2)}) copy-start(bf16[256,4096]{1,0:T(8,128)(2,1)} %queries_ref.1) | copy-start | bytes 6291460
  5.1 2.8 %collective-permute-start.1 = (bf16[256,2048]{1,0:T(8,128)(2,1)S(1)}, bf16[256,2048]{1,0:T(8,128)(2,1)S(1)}, u32[]{:S(2)}, u32[]{:S(2)}) collective-permute-start(bf16[256,2048]{1,0:T(8,128)(2,1)S(1)} %get-tuple-element.37), channel_id=1, source_target_pairs={{0,1},{1,0},{2,3},{3,2},{4,5},{5,4},{6,7},{7,6},{8,9},{9,8},{10,11... | collective-permute-start | bytes 3145736 | tf_op jit(solution)/shard_map/ppermute | solution.py:490
  5.6 3.8 %collective-permute-start.2 = (bf16[256,2048]{1,0:T(8,128)(2,1)S(1)}, bf16[256,2048]{1,0:T(8,128)(2,1)S(1)}, u32[]{:S(2)}, u32[]{:S(2)}) collective-permute-start(bf16[256,2048]{1,0:T(8,128)(2,1)S(1)} %get-tuple-element.39), channel_id=1, source_target_pairs={{0,1},{1,0},{2,3},{3,2},{4,5},{5,4},{6,7},{7,6},{8,9},{9,8},{10,11... | collective-permute-start | bytes 3145736 | tf_op jit(solution)/shard_map/ppermute | solution.py:490
  6.4 8.8 %collective-permute-start = (bf16[256,2048]{1,0:T(8,128)(2,1)S(1)}, bf16[256,2048]{1,0:T(8,128)(2,1)S(1)}, u32[]{:S(2)}, u32[]{:S(2)}) collective-permute-start(bf16[256,2048]{1,0:T(8,128)(2,1)S(1)} %get-tuple-element.35), channel_id=1, source_target_pairs={{0,1},{1,0},{2,3},{3,2},{4,5},{5,4},{6,7},{7,6},{8,9},{9,8},{10,11... | collective-permute-start | bytes 3145736 | tf_op jit(solution)/shard_map/ppermute | solution.py:490
  10.8 9.4 %collective-permute-start.7 = (s16[272,128]{1,0:T(8,128)(2,1)S(1)}, s16[272,128]{1,0:T(8,128)(2,1)S(1)}, u32[]{:S(2)}, u32[]{:S(2)}) collective-permute-start(s16[272,128]{1,0:T(8,128)(2,1)S(1)} %get-tuple-element.46), channel_id=1, source_target_pairs={{0,2},{2,0},{4,6},{6,4},{1,3},{3,1},{5,7},{7,5},{8,10},{10,8},{12,... | collective-permute-start | bytes 208904 | tf_op jit(solution)/shard_map/ppermute | solution.py:490
  13.7 6.5 %collective-permute-start.8 = (s16[272,128]{1,0:T(8,128)(2,1)S(1)}, s16[272,128]{1,0:T(8,128)(2,1)S(1)}, u32[]{:S(2)}, u32[]{:S(2)}) collective-permute-start(s16[272,128]{1,0:T(8,128)(2,1)S(1)} %get-tuple-element.47), channel_id=1, source_target_pairs={{0,4},{2,6},{4,0},{6,2},{1,5},{3,7},{5,1},{7,3},{8,12},{10,14},{12... | collective-permute-start | bytes 208904 | tf_op jit(solution)/shard_map/ppermute | solution.py:490
  15.2 5.7 %collective-permute-start.9 = (s16[272,128]{1,0:T(8,128)(2,1)S(1)}, s16[272,128]{1,0:T(8,128)(2,1)S(1)}, u32[]{:S(2)}, u32[]{:S(2)}) collective-permute-start(s16[272,128]{1,0:T(8,128)(2,1)S(1)} %get-tuple-element.48), channel_id=1, source_target_pairs={{0,6},{2,4},{4,2},{6,0},{1,7},{3,5},{5,3},{7,1},{8,14},{10,12},{12... | collective-permute-start | bytes 208904 | tf_op jit(solution)/shard_map/ppermute | solution.py:490
  15.3 13.7 %copy-start.1 = (f32[1024]{0:T(1024)S(1)}, f32[1024]{0:T(1024)}, u32[]{:S(2)}) copy-start(f32[1024]{0:T(1024)} %param.9) | copy-start | bytes 12292
  16.6 7.7 %collective-permute-start.4 = (s16[272,128]{1,0:T(8,128)(2,1)S(1)}, s16[272,128]{1,0:T(8,128)(2,1)S(1)}, u32[]{:S(2)}, u32[]{:S(2)}) collective-permute-start(s16[272,128]{1,0:T(8,128)(2,1)S(1)} %get-tuple-element.43), channel_id=1, source_target_pairs={{0,2},{2,0},{4,6},{6,4},{1,3},{3,1},{5,7},{7,5},{8,10},{10,8},{12,... | collective-permute-start | bytes 208904 | tf_op jit(solution)/shard_map/ppermute | solution.py:490
  18.6 5.7 %collective-permute-start.5 = (s16[272,128]{1,0:T(8,128)(2,1)S(1)}, s16[272,128]{1,0:T(8,128)(2,1)S(1)}, u32[]{:S(2)}, u32[]{:S(2)}) collective-permute-start(s16[272,128]{1,0:T(8,128)(2,1)S(1)} %get-tuple-element.44), channel_id=1, source_target_pairs={{0,4},{2,6},{4,0},{6,2},{1,5},{3,7},{5,1},{7,3},{8,12},{10,14},{12... | collective-permute-start | bytes 208904 | tf_op jit(solution)/shard_map/ppermute | solution.py:490
  20.1 5.2 %collective-permute-start.6 = (s16[272,128]{1,0:T(8,128)(2,1)S(1)}, s16[272,128]{1,0:T(8,128)(2,1)S(1)}, u32[]{:S(2)}, u32[]{:S(2)}) collective-permute-start(s16[272,128]{1,0:T(8,128)(2,1)S(1)} %get-tuple-element.45), channel_id=1, source_target_pairs={{0,6},{2,4},{4,2},{6,0},{1,7},{3,5},{5,3},{7,1},{8,14},{10,12},{12... | collective-permute-start | bytes 208904 | tf_op jit(solution)/shard_map/ppermute | solution.py:490
  21.0 11.7 %collective-permute-start.11 = (s16[272,128]{1,0:T(8,128)(2,1)S(1)}, s16[272,128]{1,0:T(8,128)(2,1)S(1)}, u32[]{:S(2)}, u32[]{:S(2)}) collective-permute-start(s16[272,128]{1,0:T(8,128)(2,1)S(1)} %get-tuple-element.49.refs_3_), channel_id=1, source_target_pairs={{0,8},{8,16},{16,24},{1,9},{9,17},{17,25},{2,10},{10,18},{18,26},{... | collective-permute-start | bytes 208904 | tf_op jit(solution)/shard_map/ppermute | solution.py:497
  25.5 11.8 %collective-permute-start.10 = (s16[272,128]{1,0:T(8,128)(2,1)S(1)}, s16[272,128]{1,0:T(8,128)(2,1)S(1)}, u32[]{:S(2)}, u32[]{:S(2)}) collective-permute-start(s16[272,128]{1,0:T(8,128)(2,1)S(1)} %get-tuple-element.50.refs_1_), channel_id=1, source_target_pairs={{0,8},{8,16},{16,24},{1,9},{9,17},{17,25},{2,10},{10,18},{18,26},{... | collective-permute-start | bytes 208904 | tf_op jit(solution)/shard_map/ppermute | solution.py:497
  29.0 3.7 %collective-permute-start.3 = (f32[1,1024]{1,0:T(1,128)S(1)}, f32[1,1024]{1,0:T(1,128)S(1)}, u32[]{:S(2)}, u32[]{:S(2)}) collective-permute-start(f32[1,1024]{1,0:T(1,128)S(1)} %bitcast.5), channel_id=1, source_target_pairs={{0,2},{2,0},{1,3},{3,1},{4,6},{6,4},{5,7},{7,5},{8,10},{10,8},{9,1... | collective-permute-start | bytes 12296 | tf_op jit(solution)/shard_map/ppermute | solution.py:490
  32.7 7.4 %collective-permute-start.13 = (s16[272,128]{1,0:T(8,128)(2,1)S(1)}, s16[272,128]{1,0:T(8,128)(2,1)S(1)}, u32[]{:S(2)}, u32[]{:S(2)}) collective-permute-start(s16[272,128]{1,0:T(8,128)(2,1)S(1)} %levels_so_far_0_1.1.refs_1_), channel_id=1, source_target_pairs={{0,16},{8,24},{1,17},{9,25},{2,18},{10,26},{3,19},{11,27},{4,20},{... | collective-permute-start | bytes 208904 | tf_op jit(solution)/shard_map/ppermute | solution.py:497
  37.3 5.6 %collective-permute-start.12 = (s16[272,128]{1,0:T(8,128)(2,1)S(1)}, s16[272,128]{1,0:T(8,128)(2,1)S(1)}, u32[]{:S(2)}, u32[]{:S(2)}) collective-permute-start(s16[272,128]{1,0:T(8,128)(2,1)S(1)} %levels_so_far_1_1.1.refs_0_), channel_id=1, source_target_pairs={{0,16},{8,24},{1,17},{9,25},{2,18},{10,26},{3,19},{11,27},{4,20},{... | collective-permute-start | bytes 208904 | tf_op jit(solution)/shard_map/ppermute | solution.py:497
  40.8 5.8 %collective-permute-start.17 = (s16[272,128]{1,0:T(8,128)(2,1)S(1)}, s16[272,128]{1,0:T(8,128)(2,1)S(1)}, u32[]{:S(2)}, u32[]{:S(2)}) collective-permute-start(s16[272,128]{1,0:T(8,128)(2,1)S(1)} %get-tuple-element.57), channel_id=1, source_target_pairs={{0,6},{2,4},{4,2},{6,0},{1,7},{3,5},{5,3},{7,1},{8,14},{10,12},{12... | collective-permute-start | bytes 208904 | tf_op jit(solution)/shard_map/ppermute | solution.py:490
  41.6 5.5 %collective-permute-start.16 = (s16[272,128]{1,0:T(8,128)(2,1)S(1)}, s16[272,128]{1,0:T(8,128)(2,1)S(1)}, u32[]{:S(2)}, u32[]{:S(2)}) collective-permute-start(s16[272,128]{1,0:T(8,128)(2,1)S(1)} %get-tuple-element.53.refs_5_), channel_id=1, source_target_pairs={{0,2},{2,0},{4,6},{6,4},{1,3},{3,1},{5,7},{7,5},{8,10},{10,8},{12,... | collective-permute-start | bytes 208904 | tf_op jit(solution)/shard_map/ppermute | solution.py:490
  43.6 5.7 %collective-permute-start.15 = (s16[272,128]{1,0:T(8,128)(2,1)S(1)}, s16[272,128]{1,0:T(8,128)(2,1)S(1)}, u32[]{:S(2)}, u32[]{:S(2)}) collective-permute-start(s16[272,128]{1,0:T(8,128)(2,1)S(1)} %get-tuple-element.55), channel_id=1, source_target_pairs={{0,6},{2,4},{4,2},{6,0},{1,7},{3,5},{5,3},{7,1},{8,14},{10,12},{12... | collective-permute-start | bytes 208904 | tf_op jit(solution)/shard_map/ppermute | solution.py:490
  45.1 5.4 %collective-permute-start.14 = (s16[272,128]{1,0:T(8,128)(2,1)S(1)}, s16[272,128]{1,0:T(8,128)(2,1)S(1)}, u32[]{:S(2)}, u32[]{:S(2)}) collective-permute-start(s16[272,128]{1,0:T(8,128)(2,1)S(1)} %get-tuple-element.54.refs_7_), channel_id=1, source_target_pairs={{0,2},{2,0},{4,6},{6,4},{1,3},{3,1},{5,7},{7,5},{8,10},{10,8},{12,... | collective-permute-start | bytes 208904 | tf_op jit(solution)/shard_map/ppermute | solution.py:490
  48.3 19.5 %collective-permute-start.20 = (bf16[512,512]{1,0:T(8,128)(2,1)S(1)}, bf16[512,512]{1,0:T(8,128)(2,1)S(1)}, u32[]{:S(2)}, u32[]{:S(2)}) collective-permute-start(bf16[512,512]{1,0:T(8,128)(2,1)S(1)} %attend_0_1_3.1.refs_10_), channel_id=1, source_target_pairs={{0,2},{2,0},{1,3},{3,1},{4,6},{6,4},{5,7},{7,5},{8,10},{10,8},{9,1... | collective-permute-start | bytes 1572872 | tf_op jit(solution)/shard_map/ppermute | solution.py:490
  52.4 18.2 %collective-permute-start.18 = (bf16[512,512]{1,0:T(8,128)(2,1)S(1)}, bf16[512,512]{1,0:T(8,128)(2,1)S(1)}, u32[]{:S(2)}, u32[]{:S(2)}) collective-permute-start(bf16[512,512]{1,0:T(8,128)(2,1)S(1)} %attend_1_1_3.1.refs_12_.refs_10_), channel_id=1, source_target_pairs={{0,2},{2,0},{1,3},{3,1},{4,6},{6,4},{5,7},{7,5},{8,10},{10,8},{9,1... | collective-permute-start | bytes 1572872 | tf_op jit(solution)/shard_map/ppermute | solution.py:490
  54.8 11.6 %collective-permute-start.21 = (f32[2,2,128,128]{3,2,1,0:T(8,128)S(1)}, f32[2,2,128,128]{3,2,1,0:T(8,128)S(1)}, u32[]{:S(2)}, u32[]{:S(2)}) collective-permute-start(f32[2,2,128,128]{3,2,1,0:T(8,128)S(1)} %get-tuple-element.61), channel_id=1, source_target_pairs={{0,4},{4,0},{1,5},{5,1},{2,6},{6,2},{3,7},{7,3},{8,12},{12,8},{9,1... | collective-permute-start | bytes 786440 | tf_op jit(solution)/shard_map/ppermute | solution.py:490
  55.6 7.0 %collective-permute-start.19 = (s16[528,128]{1,0:T(8,128)(2,1)S(1)}, s16[528,128]{1,0:T(8,128)(2,1)S(1)}, u32[]{:S(2)}, u32[]{:S(2)}) collective-permute-start(s16[528,128]{1,0:T(8,128)(2,1)S(1)} %get-tuple-element.59), channel_id=1, source_target_pairs={{0,4},{2,6},{4,0},{6,2},{1,5},{3,7},{5,1},{7,3},{8,12},{10,14},{12... | collective-permute-start | bytes 405512 | tf_op jit(solution)/shard_map/ppermute | solution.py:490

commit v9 on v8

--- a/solution.py
+++ b/solution.py
@@ -152,17 +152,33 @@
         scaled = jnp.clip(scaled, -TOP, TOP)
         ref[i * HD : (i + 1) * HD] = scaled.astype(jnp.int32).astype(jnp.int16)
         exponents = jnp.where(line == i, exponent, exponents)
-    ref[len(states) * HD :] = exponents.astype(jnp.int32).astype(jnp.int16)
+    ref[len(states) * HD : len(states) * HD + PAD] = exponents.astype(jnp.int32).astype(jnp.int16)
 
 
 def decoded(ref):
     count = ref.shape[0] // HD
-    exponents = ref[count * HD :].astype(jnp.int32).astype(jnp.float32)
+    exponents = ref[count * HD : count * HD + PAD].astype(jnp.int32).astype(jnp.float32)
     return [
         ref[i * HD : (i + 1) * HD].astype(jnp.int32).astype(jnp.float32)
         * jnp.exp2(exponents[i : i + 1] - 15)
         for i in range(count)
     ]
+
+
+def code_gain(gain_ref, ref):
+    line = lax.broadcasted_iota(jnp.int32, (PAD // 2, HD), 0)
+    gain = jnp.zeros((PAD // 2, HD), jnp.float32)
+    for i in range(gain_ref.shape[1] // HD):
+        gain = jnp.where(line == i, gain_ref[:, i * HD : (i + 1) * HD], gain)
+    coarse = jnp.round(gain * 2.0**12)
+    fine = jnp.round((gain - coarse * 2.0**-12) * 2.0**27)
+    planes = jnp.concatenate([coarse, fine], axis=0)
+    ref[ref.shape[0] - PAD :] = planes.astype(jnp.int32).astype(jnp.int16)
+
+
+def decoded_gain(ref):
+    planes = ref[ref.shape[0] - PAD :].astype(jnp.int32).astype(jnp.float32)
+    return planes[: PAD // 2] * 2.0**-12 + planes[PAD // 2 :] * 2.0**-27
 
 
 def plus(left, right):
@@ -177,8 +193,8 @@
     return total
 
 
-def coded_shape(heads):
-    return jax.ShapeDtypeStruct((heads * HD + PAD, HD), jnp.int16)
+def coded_shape(heads, more=0):
+    return jax.ShapeDtypeStruct((heads * HD + PAD + more, HD), jnp.int16)
 
 
 def states_shape(*lead):
@@ -192,9 +208,11 @@
     return pl.ds(pl.multiple_of(start, HD), HD)
 
 
-def chunk_states(plan, place, key, value, half, after):
+def chunk_states(plan, place, key, value, half, after, gain=None):
+    gains = [] if gain is None else [gain]
+
     def kernel(place_ref, k_ref, k_sib_ref, v_ref, v_sib_ref, *refs):
-        own_ref, first_ref, *send_refs = refs[len(after) :]
+        own_ref, first_ref, *send_refs = refs[len(gains) + len(after) :]
         is_first = jnp.full((HD, HD), place_ref[0], jnp.int32) == 0
         for offset in (*range(1, plan.plane), 0):
             states = []
@@ -206,6 +224,8 @@
                 states.append(mine + sib)
             if offset:
                 code(states, send_refs[offset - 1])
+                if gains and offset < plan.n_y:
+                    code_gain(refs[0], send_refs[offset - 1])
             else:
                 for i, state in enumerate(states):
                     own_ref[i] = state
@@ -214,15 +234,18 @@
     return pl.pallas_call(
         kernel,
         out_shape=[states_shape(plan.each), states_shape(plan.plane, plan.each)]
-        + [coded_shape(plan.each)] * (plan.plane - 1),
-        in_specs=[SMEM] + [VMEM] * 4 + [ANY] * len(after),
+        + [
+            coded_shape(plan.each, PAD if gains and o < plan.n_y else 0)
+            for o in range(1, plan.plane)
+        ],
+        in_specs=[SMEM] + [VMEM] * (4 + len(gains)) + [ANY] * len(after),
         out_specs=[VMEM] * (1 + plan.plane),
         compiler_params=params(),
         cost_estimate=cost(
             4 * plan.rows * HD * HD * heads, 8 * plan.rows * HD * heads + 6 * heads * HD * HD
         ),
         name=f"chunk_states_{half}",
-    )(place, *key, *value, *after)
+    )(place, *key, *value, *gains, *after)
 
 
 def level_states(plan, own, others, half, after):
@@ -389,14 +412,20 @@
         first_ref, gain_ref, *carry_refs = refs[n : n + 2 + len(offsets)]
         out_ref = refs[-1]
         is_second = jnp.full((HD, HD), core, jnp.int32) == 1
+        coded_gain = gain_ref.dtype == jnp.int16
+        line = lax.broadcasted_iota(jnp.int32, (PAD // 2, HD), 0)
         for piece, offset in enumerate(offsets):
             x = place_ref[1] ^ (offset // plan.n_y)
             carry_states = decoded(carry_refs[piece])
             skip = half * plan.each if len(carry_states) > plan.each else 0
             for i in range(plan.each):
                 at = owned_columns(plan, place_ref, offset, half, i)
-                start = ((half * plan.n_inner + x) * plan.each + i) * HD
-                gain = gain_ref[:, pl.ds(pl.multiple_of(start, HD), HD)]
+                head = (half * plan.n_inner + x) * plan.each + i
+                if coded_gain:
+                    gain = jnp.where(line == head, decoded_gain(gain_ref), 0.0)
+                    gain = jnp.sum(gain, axis=0, keepdims=True)
+                else:
+                    gain = gain_ref[:, pl.ds(pl.multiple_of(head * HD, HD), HD)]
                 out_at = slice(piece * plan.piece + i * HD, piece * plan.piece + (i + 1) * HD)
                 carried = carry_states[skip + i]
                 first = first_ref[offset, i]
@@ -497,7 +526,6 @@
         return lax.ppermute(array, "outer", pairs)
 
     gain = gain.reshape(1, plan.width)
-    gains = [gain] + [swap(gain, "y", o, plan.n_y) for o in range(1, plan.n_y)]
     key, key_out, value, value_out, *counts = decode(plan, place, spikes, keys, values)
     key, value = ((a, swap(b, "core", 1, CORES)) for a, b in ((key, key_out), (value, value_out)))
     query, query_out = spike_queries(plan, place, queries, counts)
@@ -506,7 +534,8 @@
     own, first, others = [], [], []
 
     def owner_stage(half, after):
-        mine, parts, *sends = chunk_states(plan, place, key, value, half, after)
+        with_gain = gain if half == 0 else None
+        mine, parts, *sends = chunk_states(plan, place, key, value, half, after, with_gain)
         own.append(mine)
         first.append(parts)
         others.append([in_level(a, o) for o, a in enumerate(sends, 1)])
@@ -523,7 +552,7 @@
             value,
             [carry[o] for o in offsets],
             first[half],
-            gains[offsets[0] % plan.n_y],
+            others[0][offsets[0] % plan.n_y - 1] if offsets[0] % plan.n_y else gain,
             half,
             offsets,
             after,
@@ -555,7 +584,6 @@
         after = [coded]
     levels = [[] for _ in halves]
     distance = 1
-    after = [*after, *gains[1:]]
     while distance < plan.n_outer:
         for half in halves:
             if distance > 1:

time: 72.2 us -> 70.3 us (0.974)
  waiting for transfers between devices: 15.9 us -> 13.4 us
    ppermute x18 -> x17, waiting for transfers between devices: 15.9 us -> 13.4 us  [swap(): return lax.ppermute(array, axes, [(i, i ^ offset) for i in range(size)])]
    ppermute x4, starting transfers between devices: 12.6 us -> 14.2 us  [to_later(): return lax.ppermute(array, 'outer', pairs)]
    ppermute x18 -> x17, starting transfers between devices: 19.2 us -> 18.1 us  [swap(): return lax.ppermute(array, axes, [(i, i ^ offset) for i in range(size)])]
  transfers between devices with their start and end apart: 22 -> 21, of which waited for: 9 -> 8; matrix products, arithmetic and copies ran while one was open for 0% -> 0% of each run, Pallas kernels for 25% -> 25%
where the time goes in v9:
time: 70.3 us; the launch traced here: 70.1 us
  starting transfers between devices  32.3 us (46%)
  Pallas kernels  23.4 us (33%)
  waiting for transfers between devices  13.4 us (19%)
  between operations  0.85 us (1%)
    ppermute x17, starting transfers between devices, swap(): return lax.ppermute(array, axes, [(i, i ^ offset) for i in range(size)])  18.1 us
    ppermute x4, starting transfers between devices, to_later(): return lax.ppermute(array, 'outer', pairs)  14.2 us
    ppermute x17, waiting for transfers between devices, swap(): return lax.ppermute(array, axes, [(i, i ^ offset) for i in range(size)])  13.4 us
    pallas_call x4, Pallas kernels, attend(): pl.pallas_call(kernel, out_shape=jax.ShapeDtypeStruct((CORES * rows, head...  6.77 us
    pallas_call x1, Pallas kernels, decode(): pl.pallas_call(kernel, out_shape=[jax.ShapeDtypeStruct((rows, plan.n_y *...  4.36 us
    pallas_call x2, Pallas kernels, assemble(): pl.pallas_call(kernel, out_shape=jax.ShapeDtypeStruct((plan.n_y * rows, p...  3.08 us
    pallas_call x2, Pallas kernels, chunk_states(): pl.pallas_call(kernel, out_shape=[states_shape(plan.each), states_shape(p...  2.72 us
    pallas_call x1, Pallas kernels, attend_local(): pl.pallas_call(kernel, out_shape=jax.ShapeDtypeStruct((CORES, rows, heads...  1.48 us
  transfers between devices with their start and end apart: 21, of which 8 were waited for; matrix products, arithmetic and copies ran while one was open for 0% of the time, Pallas kernels for 25%

profile of v9, /device:TPU:0, one launch (start us, length us, event | category | flops | bytes accessed | tf_op | source)
XLA Modules:
  0.0 70.1 jit_solution(2880179656732445284)
XLA Ops:
  0.6 0.1 pad_add_fusion.place_ref
  0.7 4.4 %decode.1 = (bf16[256,2048]{1,0:T(8,128)(2,1)S(1)}, bf16[256,2048]{1,0:T(8,128)(2,1)S(1)}, bf16[256,2048]{1,0:T(8,128)(2,1)S(1)}, bf16[256,2048]{1,0:T(8,128)(2,...) custom-call(s32[4]{0:T(128)S(1)} %pad_add_fusion.place_ref, s32[256,4096]{1,0:T(8,128)} %refs_0_.1, ...), custom_call_target="tpu_custom_call" | custom-call | flops 4194304 | bytes 14680064 | tf_op jit(solution)/shard_map/decode/pallas_call | solution.py:100
  5.1 0.5 collective-permute-start.1
  5.6 0.1 collective-permute-start.2
  5.7 0.0 copy-done
  5.7 0.8 %spike_queries.1 = (bf16[256,2048]{1,0:T(8,128)(2,1)S(1)}, bf16[256,2048]{1,0:T(8,128)(2,1)S(1)}) custom-call(s32[4]{0:T(128)S(1)} %pad_add_fusion.place_ref, bf16[256,4096]{1,0:T(8,128)(2,1)S(1)} %copy-done, bf16[256,2048]{1,0:T(8,128)(2,1)S(1)} %get-tuple-element.32.refs_0_, bf16[256,2048]{1,0:T(8,128)(2,1)S(1)} %get-tuple-element.33.refs_1_), custom_call_target="tpu_custom_call" | custom-call | flops 1048576 | bytes 6291456 | tf_op jit(solution)/shard_map/spike_queries/pallas_call | solution.py:122
  6.4 0.5 collective-permute-start
  6.9 0.9 %collective-permute-done.1.k_sib_ref.refs_3_ = bf16[256,2048]{1,0:T(8,128)(2,1)S(1)} collective-permute-done((bf16[256,2048]{1,0:T(8,128)(2,1)S(1)}, bf16[256,2048]{1,0:T(8,128)(2,1)S(1)}, u32[]{:S(2)}, u32[]{:S(2)}) %collective-permute-start.1) | collective-permute-done | bytes 1048608 | tf_op jit(solution)/shard_map/ppermute | solution.py:519
  7.9 1.5 %collective-permute-done.2.v_sib_ref.refs_5_ = bf16[256,2048]{1,0:T(8,128)(2,1)S(1)} collective-permute-done((bf16[256,2048]{1,0:T(8,128)(2,1)S(1)}, bf16[256,2048]{1,0:T(8,128)(2,1)S(1)}, u32[]{:S(2)}, u32[]{:S(2)}) %collective-permute-start.2) | collective-permute-done | bytes 1048608 | tf_op jit(solution)/shard_map/ppermute | solution.py:519
  9.4 0.0 copy-done.1
  9.4 1.4 %chunk_states_0.1 = (f32[2,128,128]{2,1,0:T(8,128)S(1)}, f32[4,2,128,128]{3,2,1,0:T(8,128)S(1)}, s16[288,128]{1,0:T(8,128)(2,1)S(1)}, s16[272,128]{1,0:T(8,128)(2,1)S(1)}, s16[272,128]{1,0:T(8,128)(2,1)S(1)}) custom-call(s32[4]{0:T(128)S(1)} %pad_add_fusion.place_ref, bf16[256,2048]{1,0:T(8,128)(2,1)S(1)} %get-tuple-element.36.k_ref.refs_2_, ...), custom_call_target="tpu_custom_call" | custom-call | flops 134217728 | bytes 2883584 | tf_op jit(solution)/shard_map/chunk_states_0/pallas_call | solution.py:234
  10.8 2.9 %collective-permute-start.7 = (s16[272,128]{1,0:T(8,128)(2,1)S(1)}, s16[272,128]{1,0:T(8,128)(2,1)S(1)}, u32[]{:S(2)}, u32[]{:S(2)}) collective-permute-start(s16[272,128]{1,0:T(8,128)(2,1)S(1)} %get-tuple-element.47), channel_id=1, source_target_pairs={{0,4},{2,6},{4,0},{6,2},{1,5},{3,7},{5,1},{7,3},{8,12},{10,14},{12... | collective-permute-start | bytes 208904 | tf_op jit(solution)/shard_map/ppermute | solution.py:519
  13.7 1.5 %collective-permute-start.3 = (s16[288,128]{1,0:T(8,128)(2,1)S(1)}, s16[288,128]{1,0:T(8,128)(2,1)S(1)}, u32[]{:S(2)}, u32[]{:S(2)}) collective-permute-start(s16[288,128]{1,0:T(8,128)(2,1)S(1)} %get-tuple-element.42), channel_id=1, source_target_pairs={{0,2},{2,0},{4,6},{6,4},{1,3},{3,1},{5,7},{7,5},{8,10},{10,8},{12,... | collective-permute-start | bytes 221192 | tf_op jit(solution)/shard_map/ppermute | solution.py:519
  15.2 0.0 collective-permute-start.8
  15.2 0.0 collective-permute-done.refs_1_.refs_4_.q_sib_ref
  15.2 1.4 %chunk_states_1.1 = (f32[2,128,128]{2,1,0:T(8,128)S(1)}, f32[4,2,128,128]{3,2,1,0:T(8,128)S(1)}, s16[272,128]{1,0:T(8,128)(2,1)S(1)}, s16[272,128]{1,0:T(8,128)(2,1)S(1)}, s16[272,128]{1,0:T(8,128)(2,1)S(1)}) custom-call(s32[4]{0:T(128)S(1)} %pad_add_fusion.place_ref, bf16[256,2048]{1,0:T(8,128)(2,1)S(1)} %get-tuple-element.36.k_ref.refs_2_, ...), custom_call_target="tpu_custom_call" | custom-call | flops 134217728 | bytes 2883584 | tf_op jit(solution)/shard_map/chunk_states_1/pallas_call | solution.py:234
  16.6 2.0 %collective-permute-start.4 = (s16[272,128]{1,0:T(8,128)(2,1)S(1)}, s16[272,128]{1,0:T(8,128)(2,1)S(1)}, u32[]{:S(2)}, u32[]{:S(2)}) collective-permute-start(s16[272,128]{1,0:T(8,128)(2,1)S(1)} %get-tuple-element.44), channel_id=1, source_target_pairs={{0,2},{2,0},{4,6},{6,4},{1,3},{3,1},{5,7},{7,5},{8,10},{10,8},{12,... | collective-permute-start | bytes 208904 | tf_op jit(solution)/shard_map/ppermute | solution.py:519
  18.6 1.5 %collective-permute-start.5 = (s16[272,128]{1,0:T(8,128)(2,1)S(1)}, s16[272,128]{1,0:T(8,128)(2,1)S(1)}, u32[]{:S(2)}, u32[]{:S(2)}) collective-permute-start(s16[272,128]{1,0:T(8,128)(2,1)S(1)} %get-tuple-element.45), channel_id=1, source_target_pairs={{0,4},{2,6},{4,0},{6,2},{1,5},{3,7},{5,1},{7,3},{8,12},{10,14},{12... | collective-permute-start | bytes 208904 | tf_op jit(solution)/shard_map/ppermute | solution.py:519
  20.1 0.0 collective-permute-done.7.refs_1_.refs_2_
  20.1 0.1 collective-permute-start.6
  20.2 0.7 collective-permute-done.8.refs_2_.refs_3_
  20.9 0.0 collective-permute-done.3.refs_0_.refs_4_.refs_7_.refs_1_
  20.9 0.1 level_states_0.1
  21.0 3.3 %collective-permute-start.10 = (s16[272,128]{1,0:T(8,128)(2,1)S(1)}, s16[272,128]{1,0:T(8,128)(2,1)S(1)}, u32[]{:S(2)}, u32[]{:S(2)}) collective-permute-start(s16[272,128]{1,0:T(8,128)(2,1)S(1)} %get-tuple-element.49.refs_3_), channel_id=1, source_target_pairs={{0,8},{8,16},{16,24},{1,9},{9,17},{17,25},{2,10},{10,18},{18,26},{... | collective-permute-start | bytes 208904 | tf_op jit(solution)/shard_map/ppermute | solution.py:526
  24.3 0.0 collective-permute-done.4.refs_0_.refs_7_
  24.3 0.0 collective-permute-done.5.refs_1_.refs_8_
  24.3 1.0 %collective-permute-done.6.refs_2_.refs_9_ = s16[272,128]{1,0:T(8,128)(2,1)S(1)} collective-permute-done((s16[272,128]{1,0:T(8,128)(2,1)S(1)}, s16[272,128]{1,0:T(8,128)(2,1)S(1)}, u32[]{:S(2)}, u32[]{:S(2)}) %collective-permute-start.6) | collective-permute-done | bytes 69664 | tf_op jit(solution)/shard_map/ppermute | solution.py:519
  25.3 0.1 level_states_1.1
  25.4 3.5 %collective-permute-start.9 = (s16[272,128]{1,0:T(8,128)(2,1)S(1)}, s16[272,128]{1,0:T(8,128)(2,1)S(1)}, u32[]{:S(2)}, u32[]{:S(2)}) collective-permute-start(s16[272,128]{1,0:T(8,128)(2,1)S(1)} %get-tuple-element.50.refs_1_), channel_id=1, source_target_pairs={{0,8},{8,16},{16,24},{1,9},{9,17},{17,25},{2,10},{10,18},{18,26},{... | collective-permute-start | bytes 208904 | tf_op jit(solution)/shard_map/ppermute | solution.py:526
  28.9 0.0 collective-permute-done.10.refs_0_.refs_3_.refs_4_
  28.9 0.1 levels_so_far_0_1.1.refs_1_
  29.0 4.5 %collective-permute-start.12 = (s16[272,128]{1,0:T(8,128)(2,1)S(1)}, s16[272,128]{1,0:T(8,128)(2,1)S(1)}, u32[]{:S(2)}, u32[]{:S(2)}) collective-permute-start(s16[272,128]{1,0:T(8,128)(2,1)S(1)} %levels_so_far_0_1.1.refs_1_), channel_id=1, source_target_pairs={{0,16},{8,24},{1,17},{9,25},{2,18},{10,26},{3,19},{11,27},{4,20},{... | collective-permute-start | bytes 208904 | tf_op jit(solution)/shard_map/ppermute | solution.py:526
  33.5 0.0 collective-permute-done.9.refs_0_.refs_3_.refs_10_
  33.5 0.1 levels_so_far_1_1.1.refs_0_
  33.6 2.9 %collective-permute-start.11 = (s16[272,128]{1,0:T(8,128)(2,1)S(1)}, s16[272,128]{1,0:T(8,128)(2,1)S(1)}, u32[]{:S(2)}, u32[]{:S(2)}) collective-permute-start(s16[272,128]{1,0:T(8,128)(2,1)S(1)} %levels_so_far_1_1.1.refs_0_), channel_id=1, source_target_pairs={{0,16},{8,24},{1,17},{9,25},{2,18},{10,26},{3,19},{11,27},{4,20},{... | collective-permute-start | bytes 208904 | tf_op jit(solution)/shard_map/ppermute | solution.py:526
  36.5 1.5 %attend_local_0_1_3.1.refs_5_.refs_2_ = f32[2,256,512]{2,1,0:T(8,128)S(1)} custom-call(s32[4]{0:T(128)S(1)} %pad_add_fusion.place_ref, bf16[256,2048]{1,0:T(8,128)(2,1)S(1)} %get-tuple-element.34.refs_1_.q_ref.refs_0_, bf16[256,2048]{1,0:T(8,128)(2,1)S(1)} %collective-permute-done.refs_1_.refs_4_.q_sib_ref, ...), custom_call_target="tpu_custom_call" | custom-call | flops 268435456 | bytes 2097152 | tf_op jit(solution)/shard_map/attend_local_0_1_3/pallas_call | solution.py:372
  38.0 0.0 collective-permute-done.12.refs_4_.refs_5_
  38.0 0.7 %carries_0.1 = (s16[272,128]{1,0:T(8,128)(2,1)S(1)}, s16[272,128]{1,0:T(8,128)(2,1)S(1)}) custom-call(s32[4]{0:T(128)S(1)} %pad_add_fusion.place_ref, f32[2,128,128]{2,1,0:T(8,128)S(1)} %get-tuple-element.40.refs_0_.own_ref, s16[288,128]{1,0:T(8,128)(2,1)S(1)} %collective-permute-done.3.refs_0_.refs_4_.refs_7_.refs_1_, ...), custom_call_target="tpu_custom_call" | custom-call | bytes 1179648 | tf_op jit(solution)/shard_map/carries_0/pallas_call | solution.py:314
  38.8 2.6 %collective-permute-start.16 = (s16[272,128]{1,0:T(8,128)(2,1)S(1)}, s16[272,128]{1,0:T(8,128)(2,1)S(1)}, u32[]{:S(2)}, u32[]{:S(2)}) collective-permute-start(s16[272,128]{1,0:T(8,128)(2,1)S(1)} %get-tuple-element.57), channel_id=1, source_target_pairs={{0,6},{2,4},{4,2},{6,0},{1,7},{3,5},{5,3},{7,1},{8,14},{10,12},{12... | collective-permute-start | bytes 208904 | tf_op jit(solution)/shard_map/ppermute | solution.py:519
  41.4 0.5 collective-permute-start.15
  41.9 0.0 collective-permute-done.11.refs_4_.refs_11_
  41.9 0.7 %carries_1.1 = (s16[272,128]{1,0:T(8,128)(2,1)S(1)}, s16[272,128]{1,0:T(8,128)(2,1)S(1)}) custom-call(s32[4]{0:T(128)S(1)} %pad_add_fusion.place_ref, f32[2,128,128]{2,1,0:T(8,128)S(1)} %get-tuple-element.43.refs_3_.own_ref.refs_6_, s16[272,128]{1,0:T(8,128)(2,1)S(1)} %collective-permute-done.4.refs_0_.refs_7_, ...), custom_call_target="tpu_custom_call" | custom-call | bytes 1179648 | tf_op jit(solution)/shard_map/carries_1/pallas_call | solution.py:314
  42.6 1.5 %collective-permute-start.14 = (s16[272,128]{1,0:T(8,128)(2,1)S(1)}, s16[272,128]{1,0:T(8,128)(2,1)S(1)}, u32[]{:S(2)}, u32[]{:S(2)}) collective-permute-start(s16[272,128]{1,0:T(8,128)(2,1)S(1)} %get-tuple-element.55), channel_id=1, source_target_pairs={{0,6},{2,4},{4,2},{6,0},{1,7},{3,5},{5,3},{7,1},{8,14},{10,12},{12... | collective-permute-start | bytes 208904 | tf_op jit(solution)/shard_map/ppermute | solution.py:519
  44.1 0.4 collective-permute-start.13
  44.6 0.0 collective-permute-done.16.refs_6_
  44.6 1.9 %collective-permute-done.15.refs_5_ = s16[272,128]{1,0:T(8,128)(2,1)S(1)} collective-permute-done((s16[272,128]{1,0:T(8,128)(2,1)S(1)}, s16[272,128]{1,0:T(8,128)(2,1)S(1)}, u32[]{:S(2)}, u32[]{:S(2)}) %collective-permute-start.15) | collective-permute-done | bytes 69664 | tf_op jit(solution)/shard_map/ppermute | solution.py:519
  46.4 1.2 %attend_0_1_3.1.refs_10_ = bf16[512,512]{1,0:T(8,128)(2,1)S(1)} custom-call(s32[4]{0:T(128)S(1)} %pad_add_fusion.place_ref, bf16[256,2048]{1,0:T(8,128)(2,1)S(1)} %get-tuple-element.34.refs_1_.q_ref.refs_0_, bf16[256,2048]{1,0:T(8,128)(2,1)S(1)} %collective-permute-done.refs_1_.refs_4_.q_sib_ref, f32[2,256,512]{2,1,0:T(8,128)S(1)} %attend_local_0_1_3.1.refs_5_.refs_2_, ...), custom_call_target="tpu_custom_call" | custom-call | flops 402653184 | bytes 2097152 | tf_op jit(solution)/shard_map/attend_0_1_3/pallas_call | solution.py:444
  47.6 0.8 %collective-permute-start.19 = (bf16[512,512]{1,0:T(8,128)(2,1)S(1)}, bf16[512,512]{1,0:T(8,128)(2,1)S(1)}, u32[]{:S(2)}, u32[]{:S(2)}) collective-permute-start(bf16[512,512]{1,0:T(8,128)(2,1)S(1)} %attend_0_1_3.1.refs_10_), channel_id=1, source_target_pairs={{0,2},{2,0},{1,3},{3,1},{4,6},{6,4},{5,7},{7,5},{8,10},{10,8},{9,1... | collective-permute-start | bytes 1572872 | tf_op jit(solution)/shard_map/ppermute | solution.py:519
  48.5 0.0 collective-permute-done.14.refs_9_
  48.5 1.1 %collective-permute-done.13.refs_8_ = s16[272,128]{1,0:T(8,128)(2,1)S(1)} collective-permute-done((s16[272,128]{1,0:T(8,128)(2,1)S(1)}, s16[272,128]{1,0:T(8,128)(2,1)S(1)}, u32[]{:S(2)}, u32[]{:S(2)}) %collective-permute-start.13) | collective-permute-done | bytes 69664 | tf_op jit(solution)/shard_map/ppermute | solution.py:519
  49.6 1.9 %attend_1_1_3.1.refs_12_.refs_10_ = bf16[512,512]{1,0:T(8,128)(2,1)S(1)} custom-call(s32[4]{0:T(128)S(1)} %pad_add_fusion.place_ref, bf16[256,2048]{1,0:T(8,128)(2,1)S(1)} %get-tuple-element.34.refs_1_.q_ref.refs_0_, bf16[256,2048]{1,0:T(8,128)(2,1)S(1)} %collective-permute-done.refs_1_.refs_4_.q_sib_ref, ...), custom_call_target="tpu_custom_call" | custom-call | flops 402653184 | bytes 2097152 | tf_op jit(solution)/shard_map/attend_1_1_3/pallas_call | solution.py:444
  51.4 0.9 %collective-permute-start.17 = (bf16[512,512]{1,0:T(8,128)(2,1)S(1)}, bf16[512,512]{1,0:T(8,128)(2,1)S(1)}, u32[]{:S(2)}, u32[]{:S(2)}) collective-permute-start(bf16[512,512]{1,0:T(8,128)(2,1)S(1)} %attend_1_1_3.1.refs_12_.refs_10_), channel_id=1, source_target_pairs={{0,2},{2,0},{1,3},{3,1},{4,6},{6,4},{5,7},{7,5},{8,10},{10,8},{9,1... | collective-permute-start | bytes 1572872 | tf_op jit(solution)/shard_map/ppermute | solution.py:519
  52.4 1.1 %own_carries.1 = (s16[528,128]{1,0:T(8,128)(2,1)S(1)}, s16[528,128]{1,0:T(8,128)(2,1)S(1)}, f32[2,2,128,128]{3,2,1,0:T(8,128)S(1)}, f32[2,2,128,128]{3,2,1,0:T(8,128)S(1)}) custom-call(s32[4]{0:T(128)S(1)} %pad_add_fusion.place_ref, f32[2,128,128]{2,1,0:T(8,128)S(1)} %get-tuple-element.40.refs_0_.own_ref, ...), custom_call_target="tpu_custom_call" | custom-call | bytes 2621440 | tf_op jit(solution)/shard_map/own_carries/pallas_call | solution.py:348
  53.5 1.2 %collective-permute-start.20 = (f32[2,2,128,128]{3,2,1,0:T(8,128)S(1)}, f32[2,2,128,128]{3,2,1,0:T(8,128)S(1)}, u32[]{:S(2)}, u32[]{:S(2)}) collective-permute-start(f32[2,2,128,128]{3,2,1,0:T(8,128)S(1)} %get-tuple-element.61), channel_id=1, source_target_pairs={{0,4},{4,0},{1,5},{5,1},{2,6},{6,2},{3,7},{7,3},{8,12},{12,8},{9,1... | collective-permute-start | bytes 786440 | tf_op jit(solution)/shard_map/ppermute | solution.py:519
  54.6 0.9 %collective-permute-start.18 = (s16[528,128]{1,0:T(8,128)(2,1)S(1)}, s16[528,128]{1,0:T(8,128)(2,1)S(1)}, u32[]{:S(2)}, u32[]{:S(2)}) collective-permute-start(s16[528,128]{1,0:T(8,128)(2,1)S(1)} %get-tuple-element.59), channel_id=1, source_target_pairs={{0,4},{2,6},{4,0},{6,2},{1,5},{3,7},{5,1},{7,3},{8,12},{10,14},{12... | collective-permute-start | bytes 405512 | tf_op jit(solution)/shard_map/ppermute | solution.py:519
  55.5 5.8 %collective-permute-done.18.refs_9_ = s16[528,128]{1,0:T(8,128)(2,1)S(1)} collective-permute-done((s16[528,128]{1,0:T(8,128)(2,1)S(1)}, s16[528,128]{1,0:T(8,128)(2,1)S(1)}, u32[]{:S(2)}, u32[]{:S(2)}) %collective-permute-start.18) | collective-permute-done | bytes 135200 | tf_op jit(solution)/shard_map/ppermute | solution.py:519
  61.3 1.9 %attend_0_0_2.1.refs_10_.refs_0_ = bf16[512,512]{1,0:T(8,128)(2,1)S(1)} custom-call(s32[4]{0:T(128)S(1)} %pad_add_fusion.place_ref, bf16[256,2048]{1,0:T(8,128)(2,1)S(1)} %get-tuple-element.34.refs_1_.q_ref.refs_0_, bf16[256,2048]{1,0:T(8,128)(2,1)S(1)} %collective-permute-done.refs_1_.refs_4_.q_sib_ref, ...), custom_call_target="tpu_custom_call" | custom-call | flops 402653184 | bytes 2097152 | tf_op jit(solution)/shard_map/attend_0_0_2/pallas_call | solution.py:444
  63.2 1.9 %attend_1_0_2.1.refs_1_ = bf16[512,512]{1,0:T(8,128)(2,1)S(1)} custom-call(s32[4]{0:T(128)S(1)} %pad_add_fusion.place_ref, bf16[256,2048]{1,0:T(8,128)(2,1)S(1)} %get-tuple-element.34.refs_1_.q_ref.refs_0_, bf16[256,2048]{1,0:T(8,128)(2,1)S(1)} %collective-permute-done.refs_1_.refs_4_.q_sib_ref, bf16[256,2048]{1,0:T(8,128)(2,1)S(1)} %get-tuple-element.36.k_ref.refs_2_, ...), custom_call_target="tpu_custom_call" | custom-call | flops 402653184 | bytes 2097152 | tf_op jit(solution)/shard_map/attend_1_0_2/pallas_call | solution.py:444
  65.1 0.0 collective-permute-done.20.refs_1_
  65.1 1.4 %assemble_cache.1 = f32[1,8,128,128]{3,2,1,0:T(8,128)} custom-call(s32[4]{0:T(128)S(1)} %pad_add_fusion.place_ref, f32[2,2,128,128]{3,2,1,0:T(8,128)S(1)} %get-tuple-element.60.refs_0_, f32[2,2,128,128]{3,2,1,0:T(8,128)S(1)} %collective-permute-done.20.refs_1_), custom_call_target="tpu_custom_call" | custom-call | tf_op jit(solution)/shard_map/assemble_cache/pallas_call | solution.py:504
  66.5 0.0 collective-permute-done.19.refs_2_
  66.5 1.7 %assemble.1.refs_1_ = bf16[1024,1024]{1,0:T(8,128)(2,1)} custom-call(s32[4]{0:T(128)S(1)} %pad_add_fusion.place_ref, bf16[512,512]{1,0:T(8,128)(2,1)S(1)} %attend_0_0_2.1.refs_10_.refs_0_, bf16[512,512]{1,0:T(8,128)(2,1)S(1)} %attend_1_0_2.1.refs_1_, bf16[512,512]{1,0:T(8,128)(2,1)S(1)} %collective-permute-done.19.refs_2_), custom_call_target="tpu_custom_call" | custom-call | tf_op jit(solution)/shard_map/assemble/pallas_call | solution.py:483
  68.2 0.5 collective-permute-done.17.refs_0_
  68.7 1.4 %finish.1 = bf16[1024,1024]{1,0:T(8,128)(2,1)} custom-call(s32[4]{0:T(128)S(1)} %pad_add_fusion.place_ref, bf16[512,512]{1,0:T(8,128)(2,1)S(1)} %collective-permute-done.17.refs_0_, bf16[1024,1024]{1,0:T(8,128)(2,1)} %assemble.1.refs_1_), custom_call_target="tpu_custom_call", output_to_operand_aliasing={{}: (2, {})} | custom-call | tf_op jit(solution)/shard_map/finish/pallas_call | solution.py:483
  (2 shorter events, 0.0 us)
Async XLA Ops:
  0.7 5.0 %copy-start = (bf16[256,4096]{1,0:T(8,128)(2,1)S(1)}, bf16[256,4096]{1,0:T(8,128)(2,1)}, u32[]{:S(2)}) copy-start(bf16[256,4096]{1,0:T(8,128)(2,1)} %queries_ref.1) | copy-start | bytes 6291460
  5.1 2.8 %collective-permute-start.1 = (bf16[256,2048]{1,0:T(8,128)(2,1)S(1)}, bf16[256,2048]{1,0:T(8,128)(2,1)S(1)}, u32[]{:S(2)}, u32[]{:S(2)}) collective-permute-start(bf16[256,2048]{1,0:T(8,128)(2,1)S(1)} %get-tuple-element.37), channel_id=1, source_target_pairs={{0,1},{1,0},{2,3},{3,2},{4,5},{5,4},{6,7},{7,6},{8,9},{9,8},{10,11... | collective-permute-start | bytes 3145736 | tf_op jit(solution)/shard_map/ppermute | solution.py:519
  5.6 3.8 %collective-permute-start.2 = (bf16[256,2048]{1,0:T(8,128)(2,1)S(1)}, bf16[256,2048]{1,0:T(8,128)(2,1)S(1)}, u32[]{:S(2)}, u32[]{:S(2)}) collective-permute-start(bf16[256,2048]{1,0:T(8,128)(2,1)S(1)} %get-tuple-element.39), channel_id=1, source_target_pairs={{0,1},{1,0},{2,3},{3,2},{4,5},{5,4},{6,7},{7,6},{8,9},{9,8},{10,11... | collective-permute-start | bytes 3145736 | tf_op jit(solution)/shard_map/ppermute | solution.py:519
  5.7 3.7 %copy-start.1 = (f32[1024]{0:T(1024)S(1)}, f32[1024]{0:T(1024)}, u32[]{:S(2)}) copy-start(f32[1024]{0:T(1024)} %param.9) | copy-start | bytes 12292
  6.4 8.8 %collective-permute-start = (bf16[256,2048]{1,0:T(8,128)(2,1)S(1)}, bf16[256,2048]{1,0:T(8,128)(2,1)S(1)}, u32[]{:S(2)}, u32[]{:S(2)}) collective-permute-start(bf16[256,2048]{1,0:T(8,128)(2,1)S(1)} %get-tuple-element.35), channel_id=1, source_target_pairs={{0,1},{1,0},{2,3},{3,2},{4,5},{5,4},{6,7},{7,6},{8,9},{9,8},{10,11... | collective-permute-start | bytes 3145736 | tf_op jit(solution)/shard_map/ppermute | solution.py:519
  10.8 9.4 %collective-permute-start.7 = (s16[272,128]{1,0:T(8,128)(2,1)S(1)}, s16[272,128]{1,0:T(8,128)(2,1)S(1)}, u32[]{:S(2)}, u32[]{:S(2)}) collective-permute-start(s16[272,128]{1,0:T(8,128)(2,1)S(1)} %get-tuple-element.47), channel_id=1, source_target_pairs={{0,4},{2,6},{4,0},{6,2},{1,5},{3,7},{5,1},{7,3},{8,12},{10,14},{12... | collective-permute-start | bytes 208904 | tf_op jit(solution)/shard_map/ppermute | solution.py:519
  13.7 7.2 %collective-permute-start.3 = (s16[288,128]{1,0:T(8,128)(2,1)S(1)}, s16[288,128]{1,0:T(8,128)(2,1)S(1)}, u32[]{:S(2)}, u32[]{:S(2)}) collective-permute-start(s16[288,128]{1,0:T(8,128)(2,1)S(1)} %get-tuple-element.42), channel_id=1, source_target_pairs={{0,2},{2,0},{4,6},{6,4},{1,3},{3,1},{5,7},{7,5},{8,10},{10,8},{12,... | collective-permute-start | bytes 221192 | tf_op jit(solution)/shard_map/ppermute | solution.py:519
  15.2 5.7 %collective-permute-start.8 = (s16[272,128]{1,0:T(8,128)(2,1)S(1)}, s16[272,128]{1,0:T(8,128)(2,1)S(1)}, u32[]{:S(2)}, u32[]{:S(2)}) collective-permute-start(s16[272,128]{1,0:T(8,128)(2,1)S(1)} %get-tuple-element.48), channel_id=1, source_target_pairs={{0,6},{2,4},{4,2},{6,0},{1,7},{3,5},{5,3},{7,1},{8,14},{10,12},{12... | collective-permute-start | bytes 208904 | tf_op jit(solution)/shard_map/ppermute | solution.py:519
  16.6 7.7 %collective-permute-start.4 = (s16[272,128]{1,0:T(8,128)(2,1)S(1)}, s16[272,128]{1,0:T(8,128)(2,1)S(1)}, u32[]{:S(2)}, u32[]{:S(2)}) collective-permute-start(s16[272,128]{1,0:T(8,128)(2,1)S(1)} %get-tuple-element.44), channel_id=1, source_target_pairs={{0,2},{2,0},{4,6},{6,4},{1,3},{3,1},{5,7},{7,5},{8,10},{10,8},{12,... | collective-permute-start | bytes 208904 | tf_op jit(solution)/shard_map/ppermute | solution.py:519
  18.6 5.7 %collective-permute-start.5 = (s16[272,128]{1,0:T(8,128)(2,1)S(1)}, s16[272,128]{1,0:T(8,128)(2,1)S(1)}, u32[]{:S(2)}, u32[]{:S(2)}) collective-permute-start(s16[272,128]{1,0:T(8,128)(2,1)S(1)} %get-tuple-element.45), channel_id=1, source_target_pairs={{0,4},{2,6},{4,0},{6,2},{1,5},{3,7},{5,1},{7,3},{8,12},{10,14},{12... | collective-permute-start | bytes 208904 | tf_op jit(solution)/shard_map/ppermute | solution.py:519
  20.1 5.2 %collective-permute-start.6 = (s16[272,128]{1,0:T(8,128)(2,1)S(1)}, s16[272,128]{1,0:T(8,128)(2,1)S(1)}, u32[]{:S(2)}, u32[]{:S(2)}) collective-permute-start(s16[272,128]{1,0:T(8,128)(2,1)S(1)} %get-tuple-element.46), channel_id=1, source_target_pairs={{0,6},{2,4},{4,2},{6,0},{1,7},{3,5},{5,3},{7,1},{8,14},{10,12},{12... | collective-permute-start | bytes 208904 | tf_op jit(solution)/shard_map/ppermute | solution.py:519
  21.0 8.0 %collective-permute-start.10 = (s16[272,128]{1,0:T(8,128)(2,1)S(1)}, s16[272,128]{1,0:T(8,128)(2,1)S(1)}, u32[]{:S(2)}, u32[]{:S(2)}) collective-permute-start(s16[272,128]{1,0:T(8,128)(2,1)S(1)} %get-tuple-element.49.refs_3_), channel_id=1, source_target_pairs={{0,8},{8,16},{16,24},{1,9},{9,17},{17,25},{2,10},{10,18},{18,26},{... | collective-permute-start | bytes 208904 | tf_op jit(solution)/shard_map/ppermute | solution.py:526
  25.4 8.1 %collective-permute-start.9 = (s16[272,128]{1,0:T(8,128)(2,1)S(1)}, s16[272,128]{1,0:T(8,128)(2,1)S(1)}, u32[]{:S(2)}, u32[]{:S(2)}) collective-permute-start(s16[272,128]{1,0:T(8,128)(2,1)S(1)} %get-tuple-element.50.refs_1_), channel_id=1, source_target_pairs={{0,8},{8,16},{16,24},{1,9},{9,17},{17,25},{2,10},{10,18},{18,26},{... | collective-permute-start | bytes 208904 | tf_op jit(solution)/shard_map/ppermute | solution.py:526
  29.0 9.0 %collective-permute-start.12 = (s16[272,128]{1,0:T(8,128)(2,1)S(1)}, s16[272,128]{1,0:T(8,128)(2,1)S(1)}, u32[]{:S(2)}, u32[]{:S(2)}) collective-permute-start(s16[272,128]{1,0:T(8,128)(2,1)S(1)} %levels_so_far_0_1.1.refs_1_), channel_id=1, source_target_pairs={{0,16},{8,24},{1,17},{9,25},{2,18},{10,26},{3,19},{11,27},{4,20},{... | collective-permute-start | bytes 208904 | tf_op jit(solution)/shard_map/ppermute | solution.py:526
  33.6 8.3 %collective-permute-start.11 = (s16[272,128]{1,0:T(8,128)(2,1)S(1)}, s16[272,128]{1,0:T(8,128)(2,1)S(1)}, u32[]{:S(2)}, u32[]{:S(2)}) collective-permute-start(s16[272,128]{1,0:T(8,128)(2,1)S(1)} %levels_so_far_1_1.1.refs_0_), channel_id=1, source_target_pairs={{0,16},{8,24},{1,17},{9,25},{2,18},{10,26},{3,19},{11,27},{4,20},{... | collective-permute-start | bytes 208904 | tf_op jit(solution)/shard_map/ppermute | solution.py:526
  38.8 5.8 %collective-permute-start.16 = (s16[272,128]{1,0:T(8,128)(2,1)S(1)}, s16[272,128]{1,0:T(8,128)(2,1)S(1)}, u32[]{:S(2)}, u32[]{:S(2)}) collective-permute-start(s16[272,128]{1,0:T(8,128)(2,1)S(1)} %get-tuple-element.57), channel_id=1, source_target_pairs={{0,6},{2,4},{4,2},{6,0},{1,7},{3,5},{5,3},{7,1},{8,14},{10,12},{12... | collective-permute-start | bytes 208904 | tf_op jit(solution)/shard_map/ppermute | solution.py:519
  41.4 5.1 %collective-permute-start.15 = (s16[272,128]{1,0:T(8,128)(2,1)S(1)}, s16[272,128]{1,0:T(8,128)(2,1)S(1)}, u32[]{:S(2)}, u32[]{:S(2)}) collective-permute-start(s16[272,128]{1,0:T(8,128)(2,1)S(1)} %get-tuple-element.53.refs_5_), channel_id=1, source_target_pairs={{0,2},{2,0},{4,6},{6,4},{1,3},{3,1},{5,7},{7,5},{8,10},{10,8},{12,... | collective-permute-start | bytes 208904 | tf_op jit(solution)/shard_map/ppermute | solution.py:519
  42.6 5.8 %collective-permute-start.14 = (s16[272,128]{1,0:T(8,128)(2,1)S(1)}, s16[272,128]{1,0:T(8,128)(2,1)S(1)}, u32[]{:S(2)}, u32[]{:S(2)}) collective-permute-start(s16[272,128]{1,0:T(8,128)(2,1)S(1)} %get-tuple-element.55), channel_id=1, source_target_pairs={{0,6},{2,4},{4,2},{6,0},{1,7},{3,5},{5,3},{7,1},{8,14},{10,12},{12... | collective-permute-start | bytes 208904 | tf_op jit(solution)/shard_map/ppermute | solution.py:519
  44.1 5.4 %collective-permute-start.13 = (s16[272,128]{1,0:T(8,128)(2,1)S(1)}, s16[272,128]{1,0:T(8,128)(2,1)S(1)}, u32[]{:S(2)}, u32[]{:S(2)}) collective-permute-start(s16[272,128]{1,0:T(8,128)(2,1)S(1)} %get-tuple-element.54.refs_7_), channel_id=1, source_target_pairs={{0,2},{2,0},{4,6},{6,4},{1,3},{3,1},{5,7},{7,5},{8,10},{10,8},{12,... | collective-permute-start | bytes 208904 | tf_op jit(solution)/shard_map/ppermute | solution.py:519
  47.6 18.9 %collective-permute-start.19 = (bf16[512,512]{1,0:T(8,128)(2,1)S(1)}, bf16[512,512]{1,0:T(8,128)(2,1)S(1)}, u32[]{:S(2)}, u32[]{:S(2)}) collective-permute-start(bf16[512,512]{1,0:T(8,128)(2,1)S(1)} %attend_0_1_3.1.refs_10_), channel_id=1, source_target_pairs={{0,2},{2,0},{1,3},{3,1},{4,6},{6,4},{5,7},{7,5},{8,10},{10,8},{9,1... | collective-permute-start | bytes 1572872 | tf_op jit(solution)/shard_map/ppermute | solution.py:519
  51.4 17.3 %collective-permute-start.17 = (bf16[512,512]{1,0:T(8,128)(2,1)S(1)}, bf16[512,512]{1,0:T(8,128)(2,1)S(1)}, u32[]{:S(2)}, u32[]{:S(2)}) collective-permute-start(bf16[512,512]{1,0:T(8,128)(2,1)S(1)} %attend_1_1_3.1.refs_12_.refs_10_), channel_id=1, source_target_pairs={{0,2},{2,0},{1,3},{3,1},{4,6},{6,4},{5,7},{7,5},{8,10},{10,8},{9,1... | collective-permute-start | bytes 1572872 | tf_op jit(solution)/shard_map/ppermute | solution.py:519
  53.5 11.7 %collective-permute-start.20 = (f32[2,2,128,128]{3,2,1,0:T(8,128)S(1)}, f32[2,2,128,128]{3,2,1,0:T(8,128)S(1)}, u32[]{:S(2)}, u32[]{:S(2)}) collective-permute-start(f32[2,2,128,128]{3,2,1,0:T(8,128)S(1)} %get-tuple-element.61), channel_id=1, source_target_pairs={{0,4},{4,0},{1,5},{5,1},{2,6},{6,2},{3,7},{7,3},{8,12},{12,8},{9,1... | collective-permute-start | bytes 786440 | tf_op jit(solution)/shard_map/ppermute | solution.py:519
  54.6 6.7 %collective-permute-start.18 = (s16[528,128]{1,0:T(8,128)(2,1)S(1)}, s16[528,128]{1,0:T(8,128)(2,1)S(1)}, u32[]{:S(2)}, u32[]{:S(2)}) collective-permute-start(s16[528,128]{1,0:T(8,128)(2,1)S(1)} %get-tuple-element.59), channel_id=1, source_target_pairs={{0,4},{2,6},{4,0},{6,2},{1,5},{3,7},{5,1},{7,3},{8,12},{10,14},{12... | collective-permute-start | bytes 405512 | tf_op jit(solution)/shard_map/ppermute | solution.py:519

commit v10 on v9

--- a/solution.py
+++ b/solution.py
@@ -208,17 +208,37 @@
     return pl.ds(pl.multiple_of(start, HD), HD)
 
 
-def chunk_states(plan, place, key, value, half, after, gain=None):
+def core_states(plan, place, key, value, after):
+    def kernel(place_ref, k_ref, v_ref, *refs):
+        for half in range(plan.halves):
+            for offset in range(plan.plane):
+                for i in range(plan.each):
+                    at = owned_columns(plan, place_ref, offset, half, i)
+                    refs[-1][half, offset, i] = contract_rows(v_ref[:, at], k_ref[:, at])
+
+    heads = plan.halves * plan.plane * plan.each
+    return pl.pallas_call(
+        kernel,
+        out_shape=states_shape(plan.halves, plan.plane, plan.each),
+        in_specs=[SMEM] + [VMEM] * 2 + [ANY] * len(after),
+        out_specs=VMEM,
+        compiler_params=params(),
+        cost_estimate=cost(2 * plan.rows * HD * HD * heads, 4 * heads * HD * (plan.rows + HD)),
+        name="core_states",
+    )(place, key, value, *after)
+
+
+def chunk_states(plan, place, mine, key_sib, value_sib, half, after, gain=None):
     gains = [] if gain is None else [gain]
 
-    def kernel(place_ref, k_ref, k_sib_ref, v_ref, v_sib_ref, *refs):
+    def kernel(place_ref, mine_ref, k_sib_ref, v_sib_ref, *refs):
         own_ref, first_ref, *send_refs = refs[len(gains) + len(after) :]
         is_first = jnp.full((HD, HD), place_ref[0], jnp.int32) == 0
         for offset in (*range(1, plan.plane), 0):
             states = []
             for i in range(plan.each):
                 at = owned_columns(plan, place_ref, offset, half, i)
-                mine = contract_rows(v_ref[:, at], k_ref[:, at])
+                mine = mine_ref[half, offset, i]
                 sib = contract_rows(v_sib_ref[:, at], k_sib_ref[:, at])
                 first_ref[offset, i] = jnp.where(is_first, mine, sib)
                 states.append(mine + sib)
@@ -238,47 +258,29 @@
             coded_shape(plan.each, PAD if gains and o < plan.n_y else 0)
             for o in range(1, plan.plane)
         ],
-        in_specs=[SMEM] + [VMEM] * (4 + len(gains)) + [ANY] * len(after),
+        in_specs=[SMEM] + [VMEM] * (3 + len(gains)) + [ANY] * len(after),
         out_specs=[VMEM] * (1 + plan.plane),
         compiler_params=params(),
         cost_estimate=cost(
-            4 * plan.rows * HD * HD * heads, 8 * plan.rows * HD * heads + 6 * heads * HD * HD
+            2 * plan.rows * HD * HD * heads, 4 * plan.rows * HD * heads + 10 * heads * HD * HD
         ),
         name=f"chunk_states_{half}",
-    )(place, *key, *value, *gains, *after)
+    )(place, mine, key_sib, value_sib, *gains, *after)
 
 
 def level_states(plan, own, others, half, after):
     def kernel(own_ref, *refs):
-        total = total_of((own_ref, *refs[: len(others)]), plan.each)
-        for i, state in enumerate(total):
-            refs[-2][i] = state
-        code(total, refs[-1])
-
-    return pl.pallas_call(
-        kernel,
-        out_shape=[states_shape(plan.each), coded_shape(plan.each)],
+        code(total_of((own_ref, *refs[: len(others)]), plan.each), refs[-1])
+
+    return pl.pallas_call(
+        kernel,
+        out_shape=coded_shape(plan.each),
         in_specs=[VMEM] * plan.plane + [ANY] * len(after),
-        out_specs=[VMEM] * 2,
+        out_specs=VMEM,
         compiler_params=params(),
         cost_estimate=cost(0, plan.plane * plan.each * HD * HD * 2),
         name=f"level_states_{half}",
     )(own, *others, *after)
-
-
-def levels_so_far(plan, total, arrived, half, after):
-    def kernel(total_ref, *refs):
-        code(total_of((total_ref, *refs[: len(arrived)]), plan.each), refs[-1])
-
-    return pl.pallas_call(
-        kernel,
-        out_shape=coded_shape(plan.each),
-        in_specs=[VMEM] * (1 + len(arrived)) + [ANY] * len(after),
-        out_specs=VMEM,
-        compiler_params=params(),
-        cost_estimate=cost(0, 2 * plan.each * HD * HD * 2),
-        name=f"levels_so_far_{half}_{len(arrived)}",
-    )(total, *arrived, *after)
 
 
 def carried(plan, place_ref, own, others, levels, offsets):
@@ -531,11 +533,12 @@
     query, query_out = spike_queries(plan, place, queries, counts)
     query = (query, swap(query_out, "core", 1, CORES))
 
+    of_core = core_states(plan, place, key[0], value[0], [query[0]])
     own, first, others = [], [], []
 
     def owner_stage(half, after):
         with_gain = gain if half == 0 else None
-        mine, parts, *sends = chunk_states(plan, place, key, value, half, after, with_gain)
+        mine, parts, *sends = chunk_states(plan, place, of_core, key[1], value[1], half, after, with_gain)
         own.append(mine)
         first.append(parts)
         others.append([in_level(a, o) for o, a in enumerate(sends, 1)])
@@ -572,25 +575,15 @@
             after = [part]
         return after
 
-    after = [query[0]]
+    after = []
     for half in halves:
         owner_stage(half, after)
         after = [own[-1], query[1]]
-    totals, sums = [], []
+    levels = []
     for half in halves:
-        total, coded = level_states(plan, own[half], others[half], half, after)
-        totals.append(total)
-        sums.append(coded)
-        after = [coded]
-    levels = [[] for _ in halves]
-    distance = 1
-    while distance < plan.n_outer:
-        for half in halves:
-            if distance > 1:
-                sums[half] = levels_so_far(plan, totals[half], levels[half], half, after)
-                after = [sums[half]]
-            levels[half].append(to_later(sums[half], distance))
-        distance *= 2
+        level = level_states(plan, own[half], others[half], half, after)
+        levels.append([to_later(level, d) for d in range(plan.n_outer - 1, 0, -1)])
+        after = [level]
     local = {}
     for y in range(1, plan.n_y):
         local[y] = attend_local(plan, place, query, key, value, 0, of_group[y], after)

time: 70.3 us -> 68.9 us (0.980)
  waiting for transfers between devices: 13.4 us -> 11.1 us
    ppermute x17, waiting for transfers between devices: 13.4 us -> 11.1 us  [swap(): return lax.ppermute(array, axes, [(i, i ^ offset) for i in range(size)])]
    ppermute x17, starting transfers between devices: 18.1 us -> 19.6 us  [swap(): return lax.ppermute(array, axes, [(i, i ^ offset) for i in range(size)])]
    pallas_call x4 -> x3, Pallas kernels: 0.33 us -> 1.56 us  [the longest x1 1.36 us: core_states(): pl.pallas_call(kernel, out_shape=states_shape(plan.halves, plan.plane, pl...]
    ppermute x4 -> x6, starting transfers between devices: 14.2 us -> 13 us  [to_later(): return lax.ppermute(array, 'outer', pairs)]
  transfers between devices with their start and end apart: 21 -> 23, of which waited for: 8 -> 6; matrix products, arithmetic and copies ran while one was open for 0% -> 0% of each run, Pallas kernels for 25% -> 27%
where the time goes in v10:
time: 68.9 us; the launch traced here: 68.7 us
  starting transfers between devices  32.6 us (47%)
  Pallas kernels  24.1 us (35%)
  waiting for transfers between devices  11.1 us (16%)
  between operations  0.87 us (1%)
    ppermute x17, starting transfers between devices, swap(): return lax.ppermute(array, axes, [(i, i ^ offset) for i in range(size)])  19.6 us
    ppermute x6, starting transfers between devices, to_later(): return lax.ppermute(array, 'outer', pairs)  13 us
    ppermute x17, waiting for transfers between devices, swap(): return lax.ppermute(array, axes, [(i, i ^ offset) for i in range(size)])  11.1 us
    pallas_call x4, Pallas kernels, attend(): pl.pallas_call(kernel, out_shape=jax.ShapeDtypeStruct((CORES * rows, head...  6.75 us
    pallas_call x1, Pallas kernels, decode(): pl.pallas_call(kernel, out_shape=[jax.ShapeDtypeStruct((rows, plan.n_y *...  4.36 us
    pallas_call x2, Pallas kernels, assemble(): pl.pallas_call(kernel, out_shape=jax.ShapeDtypeStruct((plan.n_y * rows, p...  3.08 us
    pallas_call x2, Pallas kernels, chunk_states(): pl.pallas_call(kernel, out_shape=[states_shape(plan.each), states_shape(p...  2.1 us
    pallas_call x2, Pallas kernels, carries(): pl.pallas_call(kernel, out_shape=[coded_shape(plan.each)] * len(offsets),...  1.5 us
  transfers between devices with their start and end apart: 23, of which 6 were waited for; matrix products, arithmetic and copies ran while one was open for 0% of the time, Pallas kernels for 27%

profile of v10, /device:TPU:0, one launch (start us, length us, event | category | flops | bytes accessed | tf_op | source)
XLA Modules:
  0.0 68.7 jit_solution(8120760882193922787)
XLA Ops:
  0.6 0.1 pad_add_fusion.place_ref
  0.7 4.4 %decode.1 = (bf16[256,2048]{1,0:T(8,128)(2,1)S(1)}, bf16[256,2048]{1,0:T(8,128)(2,1)S(1)}, bf16[256,2048]{1,0:T(8,128)(2,1)S(1)}, bf16[256,2048]{1,0:T(8,128)(2,...) custom-call(s32[4]{0:T(128)S(1)} %pad_add_fusion.place_ref, s32[256,4096]{1,0:T(8,128)} %refs_0_.1, ...), custom_call_target="tpu_custom_call" | custom-call | flops 4194304 | bytes 14680064 | tf_op jit(solution)/shard_map/decode/pallas_call | solution.py:100
  5.1 0.5 collective-permute-start.1
  5.6 0.1 collective-permute-start.2
  5.7 0.8 %spike_queries.1 = (bf16[256,2048]{1,0:T(8,128)(2,1)S(1)}, bf16[256,2048]{1,0:T(8,128)(2,1)S(1)}) custom-call(s32[4]{0:T(128)S(1)} %pad_add_fusion.place_ref, bf16[256,4096]{1,0:T(8,128)(2,1)S(1)} %copy-done, bf16[256,2048]{1,0:T(8,128)(2,1)S(1)} %get-tuple-element.28.refs_0_, bf16[256,2048]{1,0:T(8,128)(2,1)S(1)} %get-tuple-element.29.refs_1_), custom_call_target="tpu_custom_call" | custom-call | flops 1048576 | bytes 6291456 | tf_op jit(solution)/shard_map/spike_queries/pallas_call | solution.py:122
  6.4 0.5 collective-permute-start
  6.9 1.4 %core_states.1.mine_ref = f32[2,4,2,128,128]{4,3,2,1,0:T(8,128)S(1)} custom-call(s32[4]{0:T(128)S(1)} %pad_add_fusion.place_ref, bf16[256,2048]{1,0:T(8,128)(2,1)S(1)} %get-tuple-element.32.k_ref.refs_2_, bf16[256,2048]{1,0:T(8,128)(2,1)S(1)} %get-tuple-element.34.v_ref.refs_4_, bf16[256,2048]{1,0:T(8,128)(2,1)S(1)} %get-tuple-element.30.refs_0_.q_ref), custom_call_target="tpu_custom_call" | custom-call | flops 134217728 | bytes 3145728 | tf_op jit(solution)/shard_map/core_states/pallas_call | solution.py:220
  8.3 0.0 collective-permute-done.1.k_sib_ref.refs_3_
  8.3 1.1 %collective-permute-done.2.v_sib_ref.refs_5_ = bf16[256,2048]{1,0:T(8,128)(2,1)S(1)} collective-permute-done((bf16[256,2048]{1,0:T(8,128)(2,1)S(1)}, bf16[256,2048]{1,0:T(8,128)(2,1)S(1)}, u32[]{:S(2)}, u32[]{:S(2)}) %collective-permute-start.2) | collective-permute-done | bytes 1048608 | tf_op jit(solution)/shard_map/ppermute | solution.py:521
  9.4 1.0 %chunk_states_0.1 = (f32[2,128,128]{2,1,0:T(8,128)S(1)}, f32[4,2,128,128]{3,2,1,0:T(8,128)S(1)}, s16[288,128]{1,0:T(8,128)(2,1)S(1)}, s16[272,128]{1,0:T(8,128)(2,1)S(1)}, s16[272,128]{1,0:T(8,128)(2,1)S(1)}) custom-call(s32[4]{0:T(128)S(1)} %pad_add_fusion.place_ref, f32[2,4,2,128,128]{4,3,2,1,0:T(8,128)S(1)} %core_states.1.mine_ref, ...), custom_call_target="tpu_custom_call" | custom-call | flops 67108864 | bytes 2359296 | tf_op jit(solution)/shard_map/chunk_states_0/pallas_call | solution.py:254
  10.4 2.9 %collective-permute-start.3 = (s16[288,128]{1,0:T(8,128)(2,1)S(1)}, s16[288,128]{1,0:T(8,128)(2,1)S(1)}, u32[]{:S(2)}, u32[]{:S(2)}) collective-permute-start(s16[288,128]{1,0:T(8,128)(2,1)S(1)} %get-tuple-element.38), channel_id=1, source_target_pairs={{0,2},{2,0},{4,6},{6,4},{1,3},{3,1},{5,7},{7,5},{8,10},{10,8},{12,... | collective-permute-start | bytes 221192 | tf_op jit(solution)/shard_map/ppermute | solution.py:521
  13.4 1.5 %collective-permute-start.7 = (s16[272,128]{1,0:T(8,128)(2,1)S(1)}, s16[272,128]{1,0:T(8,128)(2,1)S(1)}, u32[]{:S(2)}, u32[]{:S(2)}) collective-permute-start(s16[272,128]{1,0:T(8,128)(2,1)S(1)} %get-tuple-element.43), channel_id=1, source_target_pairs={{0,4},{2,6},{4,0},{6,2},{1,5},{3,7},{5,1},{7,3},{8,12},{10,14},{12... | collective-permute-start | bytes 208904 | tf_op jit(solution)/shard_map/ppermute | solution.py:521
  14.9 0.0 collective-permute-start.8
  14.9 0.0 collective-permute-done.refs_1_.refs_4_.q_sib_ref
  14.9 1.0 %chunk_states_1.1 = (f32[2,128,128]{2,1,0:T(8,128)S(1)}, f32[4,2,128,128]{3,2,1,0:T(8,128)S(1)}, s16[272,128]{1,0:T(8,128)(2,1)S(1)}, s16[272,128]{1,0:T(8,128)(2,1)S(1)}, s16[272,128]{1,0:T(8,128)(2,1)S(1)}) custom-call(s32[4]{0:T(128)S(1)} %pad_add_fusion.place_ref, f32[2,4,2,128,128]{4,3,2,1,0:T(8,128)S(1)} %core_states.1.mine_ref, ...), custom_call_target="tpu_custom_call" | custom-call | flops 67108864 | bytes 2359296 | tf_op jit(solution)/shard_map/chunk_states_1/pallas_call | solution.py:254
  16.0 2.0 %collective-permute-start.4 = (s16[272,128]{1,0:T(8,128)(2,1)S(1)}, s16[272,128]{1,0:T(8,128)(2,1)S(1)}, u32[]{:S(2)}, u32[]{:S(2)}) collective-permute-start(s16[272,128]{1,0:T(8,128)(2,1)S(1)} %get-tuple-element.40), channel_id=1, source_target_pairs={{0,2},{2,0},{4,6},{6,4},{1,3},{3,1},{5,7},{7,5},{8,10},{10,8},{12,... | collective-permute-start | bytes 208904 | tf_op jit(solution)/shard_map/ppermute | solution.py:521
  18.0 1.5 %collective-permute-start.5 = (s16[272,128]{1,0:T(8,128)(2,1)S(1)}, s16[272,128]{1,0:T(8,128)(2,1)S(1)}, u32[]{:S(2)}, u32[]{:S(2)}) collective-permute-start(s16[272,128]{1,0:T(8,128)(2,1)S(1)} %get-tuple-element.41), channel_id=1, source_target_pairs={{0,4},{2,6},{4,0},{6,2},{1,5},{3,7},{5,1},{7,3},{8,12},{10,14},{12... | collective-permute-start | bytes 208904 | tf_op jit(solution)/shard_map/ppermute | solution.py:521
  19.5 0.0 collective-permute-done.7.refs_1_.refs_2_
  19.5 0.3 collective-permute-start.6
  19.8 1.0 %collective-permute-done.8.refs_2_.refs_3_ = s16[272,128]{1,0:T(8,128)(2,1)S(1)} collective-permute-done((s16[272,128]{1,0:T(8,128)(2,1)S(1)}, s16[272,128]{1,0:T(8,128)(2,1)S(1)}, u32[]{:S(2)}, u32[]{:S(2)}) %collective-permute-start.8) | collective-permute-done | bytes 69664 | tf_op jit(solution)/shard_map/ppermute | solution.py:521
  20.8 0.0 collective-permute-done.3.refs_0_.refs_4_.refs_7_.refs_1_
  20.8 0.1 level_states_0.1.refs_3_
  20.9 3.3 %collective-permute-start.14 = (s16[272,128]{1,0:T(8,128)(2,1)S(1)}, s16[272,128]{1,0:T(8,128)(2,1)S(1)}, u32[]{:S(2)}, u32[]{:S(2)}) collective-permute-start(s16[272,128]{1,0:T(8,128)(2,1)S(1)} %level_states_0.1.refs_3_), channel_id=1, source_target_pairs={{0,8},{8,16},{16,24},{1,9},{9,17},{17,25},{2,10},{10,18},{18,26},{... | collective-permute-start | bytes 208904 | tf_op jit(solution)/shard_map/ppermute | solution.py:528
  24.2 4.5 %collective-permute-start.13 = (s16[272,128]{1,0:T(8,128)(2,1)S(1)}, s16[272,128]{1,0:T(8,128)(2,1)S(1)}, u32[]{:S(2)}, u32[]{:S(2)}) collective-permute-start(s16[272,128]{1,0:T(8,128)(2,1)S(1)} %level_states_0.1.refs_3_), channel_id=1, source_target_pairs={{0,16},{8,24},{1,17},{9,25},{2,18},{10,26},{3,19},{11,27},{4,20},{... | collective-permute-start | bytes 208904 | tf_op jit(solution)/shard_map/ppermute | solution.py:528
  28.7 0.0 collective-permute-done.4.refs_0_.refs_8_
  28.7 1.3 %collective-permute-start.12 = (s16[272,128]{1,0:T(8,128)(2,1)S(1)}, s16[272,128]{1,0:T(8,128)(2,1)S(1)}, u32[]{:S(2)}, u32[]{:S(2)}) collective-permute-start(s16[272,128]{1,0:T(8,128)(2,1)S(1)} %level_states_0.1.refs_3_), channel_id=1, source_target_pairs={{0,24},{1,25},{2,26},{3,27},{4,28},{5,29},{6,30},{7,31}} | collective-permute-start | bytes 208904 | tf_op jit(solution)/shard_map/ppermute | solution.py:528
  30.0 0.0 collective-permute-done.5.refs_1_.refs_9_
  30.1 0.0 collective-permute-done.6.refs_2_.refs_10_
  30.1 0.1 level_states_1.1.refs_0_
  30.2 1.3 %collective-permute-start.11 = (s16[272,128]{1,0:T(8,128)(2,1)S(1)}, s16[272,128]{1,0:T(8,128)(2,1)S(1)}, u32[]{:S(2)}, u32[]{:S(2)}) collective-permute-start(s16[272,128]{1,0:T(8,128)(2,1)S(1)} %level_states_1.1.refs_0_), channel_id=1, source_target_pairs={{0,8},{8,16},{16,24},{1,9},{9,17},{17,25},{2,10},{10,18},{18,26},{... | collective-permute-start | bytes 208904 | tf_op jit(solution)/shard_map/ppermute | solution.py:528
  31.5 1.3 %collective-permute-start.10 = (s16[272,128]{1,0:T(8,128)(2,1)S(1)}, s16[272,128]{1,0:T(8,128)(2,1)S(1)}, u32[]{:S(2)}, u32[]{:S(2)}) collective-permute-start(s16[272,128]{1,0:T(8,128)(2,1)S(1)} %level_states_1.1.refs_0_), channel_id=1, source_target_pairs={{0,16},{8,24},{1,17},{9,25},{2,18},{10,26},{3,19},{11,27},{4,20},{... | collective-permute-start | bytes 208904 | tf_op jit(solution)/shard_map/ppermute | solution.py:528
  32.8 0.0 collective-permute-done.14.refs_5_.refs_6_
  32.8 1.3 %collective-permute-start.9 = (s16[272,128]{1,0:T(8,128)(2,1)S(1)}, s16[272,128]{1,0:T(8,128)(2,1)S(1)}, u32[]{:S(2)}, u32[]{:S(2)}) collective-permute-start(s16[272,128]{1,0:T(8,128)(2,1)S(1)} %level_states_1.1.refs_0_), channel_id=1, source_target_pairs={{0,24},{1,25},{2,26},{3,27},{4,28},{5,29},{6,30},{7,31}} | collective-permute-start | bytes 208904 | tf_op jit(solution)/shard_map/ppermute | solution.py:528
  34.1 1.5 %attend_local_0_1_3.1.refs_6_.refs_2_ = f32[2,256,512]{2,1,0:T(8,128)S(1)} custom-call(s32[4]{0:T(128)S(1)} %pad_add_fusion.place_ref, bf16[256,2048]{1,0:T(8,128)(2,1)S(1)} %get-tuple-element.30.refs_0_.q_ref, bf16[256,2048]{1,0:T(8,128)(2,1)S(1)} %collective-permute-done.refs_1_.refs_4_.q_sib_ref, bf16[256,2048]{1,0:T(8,128)(2,1)S(1)} %get-tuple-element.32.k_ref.refs_2_, ...), custom_call_target="tpu_custom_call" | custom-call | flops 268435456 | bytes 2097152 | tf_op jit(solution)/shard_map/attend_local_0_1_3/pallas_call | solution.py:374
  35.6 0.0 collective-permute-done.13.refs_4_.refs_5_
  35.6 0.0 collective-permute-done.12.refs_3_.refs_4_
  35.6 0.7 %carries_0.1 = (s16[272,128]{1,0:T(8,128)(2,1)S(1)}, s16[272,128]{1,0:T(8,128)(2,1)S(1)}) custom-call(s32[4]{0:T(128)S(1)} %pad_add_fusion.place_ref, f32[2,128,128]{2,1,0:T(8,128)S(1)} %get-tuple-element.36.refs_0_.own_ref, s16[288,128]{1,0:T(8,128)(2,1)S(1)} %collective-permute-done.3.refs_0_.refs_4_.refs_7_.refs_1_, ...), custom_call_target="tpu_custom_call" | custom-call | bytes 1245184 | tf_op jit(solution)/shard_map/carries_0/pallas_call | solution.py:316
  36.4 1.8 %collective-permute-start.18 = (s16[272,128]{1,0:T(8,128)(2,1)S(1)}, s16[272,128]{1,0:T(8,128)(2,1)S(1)}, u32[]{:S(2)}, u32[]{:S(2)}) collective-permute-start(s16[272,128]{1,0:T(8,128)(2,1)S(1)} %get-tuple-element.49), channel_id=1, source_target_pairs={{0,6},{2,4},{4,2},{6,0},{1,7},{3,5},{5,3},{7,1},{8,14},{10,12},{12... | collective-permute-start | bytes 208904 | tf_op jit(solution)/shard_map/ppermute | solution.py:521
  38.2 0.5 collective-permute-start.17
  38.7 0.0 collective-permute-done.11.refs_5_.refs_13_
  38.7 0.0 collective-permute-done.10.refs_4_.refs_12_
  38.7 0.0 collective-permute-done.9.refs_3_.refs_11_
  38.7 0.8 %carries_1.1 = (s16[272,128]{1,0:T(8,128)(2,1)S(1)}, s16[272,128]{1,0:T(8,128)(2,1)S(1)}) custom-call(s32[4]{0:T(128)S(1)} %pad_add_fusion.place_ref, f32[2,128,128]{2,1,0:T(8,128)S(1)} %get-tuple-element.39.refs_3_.own_ref.refs_7_, s16[272,128]{1,0:T(8,128)(2,1)S(1)} %collective-permute-done.4.refs_0_.refs_8_, ...), custom_call_target="tpu_custom_call" | custom-call | bytes 1245184 | tf_op jit(solution)/shard_map/carries_1/pallas_call | solution.py:316
  39.5 1.6 %collective-permute-start.16 = (s16[272,128]{1,0:T(8,128)(2,1)S(1)}, s16[272,128]{1,0:T(8,128)(2,1)S(1)}, u32[]{:S(2)}, u32[]{:S(2)}) collective-permute-start(s16[272,128]{1,0:T(8,128)(2,1)S(1)} %get-tuple-element.47), channel_id=1, source_target_pairs={{0,6},{2,4},{4,2},{6,0},{1,7},{3,5},{5,3},{7,1},{8,14},{10,12},{12... | collective-permute-start | bytes 208904 | tf_op jit(solution)/shard_map/ppermute | solution.py:521
  41.1 1.2 %collective-permute-start.15 = (s16[272,128]{1,0:T(8,128)(2,1)S(1)}, s16[272,128]{1,0:T(8,128)(2,1)S(1)}, u32[]{:S(2)}, u32[]{:S(2)}) collective-permute-start(s16[272,128]{1,0:T(8,128)(2,1)S(1)} %get-tuple-element.46.refs_7_), channel_id=1, source_target_pairs={{0,2},{2,0},{4,6},{6,4},{1,3},{3,1},{5,7},{7,5},{8,10},{10,8},{12,... | collective-permute-start | bytes 208904 | tf_op jit(solution)/shard_map/ppermute | solution.py:521
  42.2 0.0 collective-permute-done.18.refs_6_
  42.2 1.2 %collective-permute-done.17.refs_5_ = s16[272,128]{1,0:T(8,128)(2,1)S(1)} collective-permute-done((s16[272,128]{1,0:T(8,128)(2,1)S(1)}, s16[272,128]{1,0:T(8,128)(2,1)S(1)}, u32[]{:S(2)}, u32[]{:S(2)}) %collective-permute-start.17) | collective-permute-done | bytes 69664 | tf_op jit(solution)/shard_map/ppermute | solution.py:521
  43.5 1.2 %attend_0_1_3.1.refs_10_ = bf16[512,512]{1,0:T(8,128)(2,1)S(1)} custom-call(s32[4]{0:T(128)S(1)} %pad_add_fusion.place_ref, bf16[256,2048]{1,0:T(8,128)(2,1)S(1)} %get-tuple-element.30.refs_0_.q_ref, bf16[256,2048]{1,0:T(8,128)(2,1)S(1)} %collective-permute-done.refs_1_.refs_4_.q_sib_ref, f32[2,256,512]{2,1,0:T(8,128)S(1)} %attend_local_0_1_3.1.refs_6_.refs_2_, ...), custom_call_target="tpu_custom_call" | custom-call | flops 402653184 | bytes 2097152 | tf_op jit(solution)/shard_map/attend_0_1_3/pallas_call | solution.py:446
  44.6 1.4 %collective-permute-start.21 = (bf16[512,512]{1,0:T(8,128)(2,1)S(1)}, bf16[512,512]{1,0:T(8,128)(2,1)S(1)}, u32[]{:S(2)}, u32[]{:S(2)}) collective-permute-start(bf16[512,512]{1,0:T(8,128)(2,1)S(1)} %attend_0_1_3.1.refs_10_), channel_id=1, source_target_pairs={{0,2},{2,0},{1,3},{3,1},{4,6},{6,4},{5,7},{7,5},{8,10},{10,8},{9,1... | collective-permute-start | bytes 1572872 | tf_op jit(solution)/shard_map/ppermute | solution.py:521
  46.1 0.0 collective-permute-done.16.refs_9_
  46.1 0.4 collective-permute-done.15.refs_8_
  46.4 1.9 %attend_1_1_3.1.refs_14_.refs_10_ = bf16[512,512]{1,0:T(8,128)(2,1)S(1)} custom-call(s32[4]{0:T(128)S(1)} %pad_add_fusion.place_ref, bf16[256,2048]{1,0:T(8,128)(2,1)S(1)} %get-tuple-element.30.refs_0_.q_ref, bf16[256,2048]{1,0:T(8,128)(2,1)S(1)} %collective-permute-done.refs_1_.refs_4_.q_sib_ref, bf16[256,2048]{1,0:T(8,128)(2,1)S(1)} %get-tuple-element.32.k_ref.refs_2_, ...), custom_call_target="tpu_custom_call" | custom-call | flops 402653184 | bytes 2097152 | tf_op jit(solution)/shard_map/attend_1_1_3/pallas_call | solution.py:446
  48.3 1.6 %collective-permute-start.19 = (bf16[512,512]{1,0:T(8,128)(2,1)S(1)}, bf16[512,512]{1,0:T(8,128)(2,1)S(1)}, u32[]{:S(2)}, u32[]{:S(2)}) collective-permute-start(bf16[512,512]{1,0:T(8,128)(2,1)S(1)} %attend_1_1_3.1.refs_14_.refs_10_), channel_id=1, source_target_pairs={{0,2},{2,0},{1,3},{3,1},{4,6},{6,4},{5,7},{7,5},{8,10},{10,8},{9,1... | collective-permute-start | bytes 1572872 | tf_op jit(solution)/shard_map/ppermute | solution.py:521
  49.9 1.1 %own_carries.1 = (s16[528,128]{1,0:T(8,128)(2,1)S(1)}, s16[528,128]{1,0:T(8,128)(2,1)S(1)}, f32[2,2,128,128]{3,2,1,0:T(8,128)S(1)}, f32[2,2,128,128]{3,2,1,0:T(8,128)S(1)}) custom-call(s32[4]{0:T(128)S(1)} %pad_add_fusion.place_ref, f32[2,128,128]{2,1,0:T(8,128)S(1)} %get-tuple-element.36.refs_0_.own_ref, ...), custom_call_target="tpu_custom_call" | custom-call | bytes 2621440 | tf_op jit(solution)/shard_map/own_carries/pallas_call | solution.py:350
  51.0 0.6 collective-permute-start.22
  51.6 1.5 %collective-permute-start.20 = (s16[528,128]{1,0:T(8,128)(2,1)S(1)}, s16[528,128]{1,0:T(8,128)(2,1)S(1)}, u32[]{:S(2)}, u32[]{:S(2)}) collective-permute-start(s16[528,128]{1,0:T(8,128)(2,1)S(1)} %get-tuple-element.51), channel_id=1, source_target_pairs={{0,4},{2,6},{4,0},{6,2},{1,5},{3,7},{5,1},{7,3},{8,12},{10,14},{12... | collective-permute-start | bytes 405512 | tf_op jit(solution)/shard_map/ppermute | solution.py:521
  53.1 5.8 %collective-permute-done.20.refs_9_ = s16[528,128]{1,0:T(8,128)(2,1)S(1)} collective-permute-done((s16[528,128]{1,0:T(8,128)(2,1)S(1)}, s16[528,128]{1,0:T(8,128)(2,1)S(1)}, u32[]{:S(2)}, u32[]{:S(2)}) %collective-permute-start.20) | collective-permute-done | bytes 135200 | tf_op jit(solution)/shard_map/ppermute | solution.py:521
  58.9 1.9 %attend_0_0_2.1.refs_10_.refs_0_ = bf16[512,512]{1,0:T(8,128)(2,1)S(1)} custom-call(s32[4]{0:T(128)S(1)} %pad_add_fusion.place_ref, bf16[256,2048]{1,0:T(8,128)(2,1)S(1)} %get-tuple-element.30.refs_0_.q_ref, bf16[256,2048]{1,0:T(8,128)(2,1)S(1)} %collective-permute-done.refs_1_.refs_4_.q_sib_ref, bf16[256,2048]{1,0:T(8,128)(2,1)S(1)} %get-tuple-element.32.k_ref.refs_2_, ...), custom_call_target="tpu_custom_call" | custom-call | flops 402653184 | bytes 2097152 | tf_op jit(solution)/shard_map/attend_0_0_2/pallas_call | solution.py:446
  60.7 1.9 %attend_1_0_2.1.refs_1_ = bf16[512,512]{1,0:T(8,128)(2,1)S(1)} custom-call(s32[4]{0:T(128)S(1)} %pad_add_fusion.place_ref, bf16[256,2048]{1,0:T(8,128)(2,1)S(1)} %get-tuple-element.30.refs_0_.q_ref, bf16[256,2048]{1,0:T(8,128)(2,1)S(1)} %collective-permute-done.refs_1_.refs_4_.q_sib_ref, bf16[256,2048]{1,0:T(8,128)(2,1)S(1)} %get-tuple-element.32.k_ref.refs_2_, ...), custom_call_target="tpu_custom_call" | custom-call | flops 402653184 | bytes 2097152 | tf_op jit(solution)/shard_map/attend_1_0_2/pallas_call | solution.py:446
  62.6 1.4 %assemble_cache.1 = f32[1,8,128,128]{3,2,1,0:T(8,128)} custom-call(s32[4]{0:T(128)S(1)} %pad_add_fusion.place_ref, f32[2,2,128,128]{3,2,1,0:T(8,128)S(1)} %get-tuple-element.52.refs_0_, f32[2,2,128,128]{3,2,1,0:T(8,128)S(1)} %collective-permute-done.22.refs_1_), custom_call_target="tpu_custom_call" | custom-call | tf_op jit(solution)/shard_map/assemble_cache/pallas_call | solution.py:506
  64.0 0.0 collective-permute-done.21.refs_2_
  64.0 1.7 %assemble.1.refs_1_ = bf16[1024,1024]{1,0:T(8,128)(2,1)} custom-call(s32[4]{0:T(128)S(1)} %pad_add_fusion.place_ref, bf16[512,512]{1,0:T(8,128)(2,1)S(1)} %attend_0_0_2.1.refs_10_.refs_0_, bf16[512,512]{1,0:T(8,128)(2,1)S(1)} %attend_1_0_2.1.refs_1_, bf16[512,512]{1,0:T(8,128)(2,1)S(1)} %collective-permute-done.21.refs_2_), custom_call_target="tpu_custom_call" | custom-call | tf_op jit(solution)/shard_map/assemble/pallas_call | solution.py:485
  65.8 1.6 %collective-permute-done.19.refs_0_ = bf16[512,512]{1,0:T(8,128)(2,1)S(1)} collective-permute-done((bf16[512,512]{1,0:T(8,128)(2,1)S(1)}, bf16[512,512]{1,0:T(8,128)(2,1)S(1)}, u32[]{:S(2)}, u32[]{:S(2)}) %collective-permute-start.19) | collective-permute-done | bytes 524320 | tf_op jit(solution)/shard_map/ppermute | solution.py:521
  67.3 1.4 %finish.1 = bf16[1024,1024]{1,0:T(8,128)(2,1)} custom-call(s32[4]{0:T(128)S(1)} %pad_add_fusion.place_ref, bf16[512,512]{1,0:T(8,128)(2,1)S(1)} %collective-permute-done.19.refs_0_, bf16[1024,1024]{1,0:T(8,128)(2,1)} %assemble.1.refs_1_), custom_call_target="tpu_custom_call", output_to_operand_aliasing={{}: (2, {})} | custom-call | tf_op jit(solution)/shard_map/finish/pallas_call | solution.py:485
  (5 shorter events, 0.0 us)
Async XLA Ops:
  0.7 5.0 %copy-start = (bf16[256,4096]{1,0:T(8,128)(2,1)S(1)}, bf16[256,4096]{1,0:T(8,128)(2,1)}, u32[]{:S(2)}) copy-start(bf16[256,4096]{1,0:T(8,128)(2,1)} %queries_ref.1) | copy-start | bytes 6291460
  5.1 3.2 %collective-permute-start.1 = (bf16[256,2048]{1,0:T(8,128)(2,1)S(1)}, bf16[256,2048]{1,0:T(8,128)(2,1)S(1)}, u32[]{:S(2)}, u32[]{:S(2)}) collective-permute-start(bf16[256,2048]{1,0:T(8,128)(2,1)S(1)} %get-tuple-element.33), channel_id=1, source_target_pairs={{0,1},{1,0},{2,3},{3,2},{4,5},{5,4},{6,7},{7,6},{8,9},{9,8},{10,11... | collective-permute-start | bytes 3145736 | tf_op jit(solution)/shard_map/ppermute | solution.py:521
  5.6 3.8 %collective-permute-start.2 = (bf16[256,2048]{1,0:T(8,128)(2,1)S(1)}, bf16[256,2048]{1,0:T(8,128)(2,1)S(1)}, u32[]{:S(2)}, u32[]{:S(2)}) collective-permute-start(bf16[256,2048]{1,0:T(8,128)(2,1)S(1)} %get-tuple-element.35), channel_id=1, source_target_pairs={{0,1},{1,0},{2,3},{3,2},{4,5},{5,4},{6,7},{7,6},{8,9},{9,8},{10,11... | collective-permute-start | bytes 3145736 | tf_op jit(solution)/shard_map/ppermute | solution.py:521
  6.4 8.5 %collective-permute-start = (bf16[256,2048]{1,0:T(8,128)(2,1)S(1)}, bf16[256,2048]{1,0:T(8,128)(2,1)S(1)}, u32[]{:S(2)}, u32[]{:S(2)}) collective-permute-start(bf16[256,2048]{1,0:T(8,128)(2,1)S(1)} %get-tuple-element.31), channel_id=1, source_target_pairs={{0,1},{1,0},{2,3},{3,2},{4,5},{5,4},{6,7},{7,6},{8,9},{9,8},{10,11... | collective-permute-start | bytes 3145736 | tf_op jit(solution)/shard_map/ppermute | solution.py:521
  6.9 2.5 %copy-start.1 = (f32[1024]{0:T(1024)S(1)}, f32[1024]{0:T(1024)}, u32[]{:S(2)}) copy-start(f32[1024]{0:T(1024)} %param.9) | copy-start | bytes 12292
  10.4 10.3 %collective-permute-start.3 = (s16[288,128]{1,0:T(8,128)(2,1)S(1)}, s16[288,128]{1,0:T(8,128)(2,1)S(1)}, u32[]{:S(2)}, u32[]{:S(2)}) collective-permute-start(s16[288,128]{1,0:T(8,128)(2,1)S(1)} %get-tuple-element.38), channel_id=1, source_target_pairs={{0,2},{2,0},{4,6},{6,4},{1,3},{3,1},{5,7},{7,5},{8,10},{10,8},{12,... | collective-permute-start | bytes 221192 | tf_op jit(solution)/shard_map/ppermute | solution.py:521
  13.4 6.1 %collective-permute-start.7 = (s16[272,128]{1,0:T(8,128)(2,1)S(1)}, s16[272,128]{1,0:T(8,128)(2,1)S(1)}, u32[]{:S(2)}, u32[]{:S(2)}) collective-permute-start(s16[272,128]{1,0:T(8,128)(2,1)S(1)} %get-tuple-element.43), channel_id=1, source_target_pairs={{0,4},{2,6},{4,0},{6,2},{1,5},{3,7},{5,1},{7,3},{8,12},{10,14},{12... | collective-permute-start | bytes 208904 | tf_op jit(solution)/shard_map/ppermute | solution.py:521
  14.9 5.9 %collective-permute-start.8 = (s16[272,128]{1,0:T(8,128)(2,1)S(1)}, s16[272,128]{1,0:T(8,128)(2,1)S(1)}, u32[]{:S(2)}, u32[]{:S(2)}) collective-permute-start(s16[272,128]{1,0:T(8,128)(2,1)S(1)} %get-tuple-element.44), channel_id=1, source_target_pairs={{0,6},{2,4},{4,2},{6,0},{1,7},{3,5},{5,3},{7,1},{8,14},{10,12},{12... | collective-permute-start | bytes 208904 | tf_op jit(solution)/shard_map/ppermute | solution.py:521
  16.0 12.7 %collective-permute-start.4 = (s16[272,128]{1,0:T(8,128)(2,1)S(1)}, s16[272,128]{1,0:T(8,128)(2,1)S(1)}, u32[]{:S(2)}, u32[]{:S(2)}) collective-permute-start(s16[272,128]{1,0:T(8,128)(2,1)S(1)} %get-tuple-element.40), channel_id=1, source_target_pairs={{0,2},{2,0},{4,6},{6,4},{1,3},{3,1},{5,7},{7,5},{8,10},{10,8},{12,... | collective-permute-start | bytes 208904 | tf_op jit(solution)/shard_map/ppermute | solution.py:521
  18.0 12.0 %collective-permute-start.5 = (s16[272,128]{1,0:T(8,128)(2,1)S(1)}, s16[272,128]{1,0:T(8,128)(2,1)S(1)}, u32[]{:S(2)}, u32[]{:S(2)}) collective-permute-start(s16[272,128]{1,0:T(8,128)(2,1)S(1)} %get-tuple-element.41), channel_id=1, source_target_pairs={{0,4},{2,6},{4,0},{6,2},{1,5},{3,7},{5,1},{7,3},{8,12},{10,14},{12... | collective-permute-start | bytes 208904 | tf_op jit(solution)/shard_map/ppermute | solution.py:521
  19.5 10.6 %collective-permute-start.6 = (s16[272,128]{1,0:T(8,128)(2,1)S(1)}, s16[272,128]{1,0:T(8,128)(2,1)S(1)}, u32[]{:S(2)}, u32[]{:S(2)}) collective-permute-start(s16[272,128]{1,0:T(8,128)(2,1)S(1)} %get-tuple-element.42), channel_id=1, source_target_pairs={{0,6},{2,4},{4,2},{6,0},{1,7},{3,5},{5,3},{7,1},{8,14},{10,12},{12... | collective-permute-start | bytes 208904 | tf_op jit(solution)/shard_map/ppermute | solution.py:521
  20.9 11.9 %collective-permute-start.14 = (s16[272,128]{1,0:T(8,128)(2,1)S(1)}, s16[272,128]{1,0:T(8,128)(2,1)S(1)}, u32[]{:S(2)}, u32[]{:S(2)}) collective-permute-start(s16[272,128]{1,0:T(8,128)(2,1)S(1)} %level_states_0.1.refs_3_), channel_id=1, source_target_pairs={{0,8},{8,16},{16,24},{1,9},{9,17},{17,25},{2,10},{10,18},{18,26},{... | collective-permute-start | bytes 208904 | tf_op jit(solution)/shard_map/ppermute | solution.py:528
  24.2 11.4 %collective-permute-start.13 = (s16[272,128]{1,0:T(8,128)(2,1)S(1)}, s16[272,128]{1,0:T(8,128)(2,1)S(1)}, u32[]{:S(2)}, u32[]{:S(2)}) collective-permute-start(s16[272,128]{1,0:T(8,128)(2,1)S(1)} %level_states_0.1.refs_3_), channel_id=1, source_target_pairs={{0,16},{8,24},{1,17},{9,25},{2,18},{10,26},{3,19},{11,27},{4,20},{... | collective-permute-start | bytes 208904 | tf_op jit(solution)/shard_map/ppermute | solution.py:528
  28.7 6.9 %collective-permute-start.12 = (s16[272,128]{1,0:T(8,128)(2,1)S(1)}, s16[272,128]{1,0:T(8,128)(2,1)S(1)}, u32[]{:S(2)}, u32[]{:S(2)}) collective-permute-start(s16[272,128]{1,0:T(8,128)(2,1)S(1)} %level_states_0.1.refs_3_), channel_id=1, source_target_pairs={{0,24},{1,25},{2,26},{3,27},{4,28},{5,29},{6,30},{7,31}} | collective-permute-start | bytes 208904 | tf_op jit(solution)/shard_map/ppermute | solution.py:528
  30.2 8.6 %collective-permute-start.11 = (s16[272,128]{1,0:T(8,128)(2,1)S(1)}, s16[272,128]{1,0:T(8,128)(2,1)S(1)}, u32[]{:S(2)}, u32[]{:S(2)}) collective-permute-start(s16[272,128]{1,0:T(8,128)(2,1)S(1)} %level_states_1.1.refs_0_), channel_id=1, source_target_pairs={{0,8},{8,16},{16,24},{1,9},{9,17},{17,25},{2,10},{10,18},{18,26},{... | collective-permute-start | bytes 208904 | tf_op jit(solution)/shard_map/ppermute | solution.py:528
  31.5 7.3 %collective-permute-start.10 = (s16[272,128]{1,0:T(8,128)(2,1)S(1)}, s16[272,128]{1,0:T(8,128)(2,1)S(1)}, u32[]{:S(2)}, u32[]{:S(2)}) collective-permute-start(s16[272,128]{1,0:T(8,128)(2,1)S(1)} %level_states_1.1.refs_0_), channel_id=1, source_target_pairs={{0,16},{8,24},{1,17},{9,25},{2,18},{10,26},{3,19},{11,27},{4,20},{... | collective-permute-start | bytes 208904 | tf_op jit(solution)/shard_map/ppermute | solution.py:528
  32.8 5.9 %collective-permute-start.9 = (s16[272,128]{1,0:T(8,128)(2,1)S(1)}, s16[272,128]{1,0:T(8,128)(2,1)S(1)}, u32[]{:S(2)}, u32[]{:S(2)}) collective-permute-start(s16[272,128]{1,0:T(8,128)(2,1)S(1)} %level_states_1.1.refs_0_), channel_id=1, source_target_pairs={{0,24},{1,25},{2,26},{3,27},{4,28},{5,29},{6,30},{7,31}} | collective-permute-start | bytes 208904 | tf_op jit(solution)/shard_map/ppermute | solution.py:528
  36.4 5.9 %collective-permute-start.18 = (s16[272,128]{1,0:T(8,128)(2,1)S(1)}, s16[272,128]{1,0:T(8,128)(2,1)S(1)}, u32[]{:S(2)}, u32[]{:S(2)}) collective-permute-start(s16[272,128]{1,0:T(8,128)(2,1)S(1)} %get-tuple-element.49), channel_id=1, source_target_pairs={{0,6},{2,4},{4,2},{6,0},{1,7},{3,5},{5,3},{7,1},{8,14},{10,12},{12... | collective-permute-start | bytes 208904 | tf_op jit(solution)/shard_map/ppermute | solution.py:521
  38.2 5.2 %collective-permute-start.17 = (s16[272,128]{1,0:T(8,128)(2,1)S(1)}, s16[272,128]{1,0:T(8,128)(2,1)S(1)}, u32[]{:S(2)}, u32[]{:S(2)}) collective-permute-start(s16[272,128]{1,0:T(8,128)(2,1)S(1)} %get-tuple-element.45.refs_6_), channel_id=1, source_target_pairs={{0,2},{2,0},{4,6},{6,4},{1,3},{3,1},{5,7},{7,5},{8,10},{10,8},{12,... | collective-permute-start | bytes 208904 | tf_op jit(solution)/shard_map/ppermute | solution.py:521
  39.5 6.6 %collective-permute-start.16 = (s16[272,128]{1,0:T(8,128)(2,1)S(1)}, s16[272,128]{1,0:T(8,128)(2,1)S(1)}, u32[]{:S(2)}, u32[]{:S(2)}) collective-permute-start(s16[272,128]{1,0:T(8,128)(2,1)S(1)} %get-tuple-element.47), channel_id=1, source_target_pairs={{0,6},{2,4},{4,2},{6,0},{1,7},{3,5},{5,3},{7,1},{8,14},{10,12},{12... | collective-permute-start | bytes 208904 | tf_op jit(solution)/shard_map/ppermute | solution.py:521
  41.1 5.4 %collective-permute-start.15 = (s16[272,128]{1,0:T(8,128)(2,1)S(1)}, s16[272,128]{1,0:T(8,128)(2,1)S(1)}, u32[]{:S(2)}, u32[]{:S(2)}) collective-permute-start(s16[272,128]{1,0:T(8,128)(2,1)S(1)} %get-tuple-element.46.refs_7_), channel_id=1, source_target_pairs={{0,2},{2,0},{4,6},{6,4},{1,3},{3,1},{5,7},{7,5},{8,10},{10,8},{12,... | collective-permute-start | bytes 208904 | tf_op jit(solution)/shard_map/ppermute | solution.py:521
  44.6 19.4 %collective-permute-start.21 = (bf16[512,512]{1,0:T(8,128)(2,1)S(1)}, bf16[512,512]{1,0:T(8,128)(2,1)S(1)}, u32[]{:S(2)}, u32[]{:S(2)}) collective-permute-start(bf16[512,512]{1,0:T(8,128)(2,1)S(1)} %attend_0_1_3.1.refs_10_), channel_id=1, source_target_pairs={{0,2},{2,0},{1,3},{3,1},{4,6},{6,4},{5,7},{7,5},{8,10},{10,8},{9,1... | collective-permute-start | bytes 1572872 | tf_op jit(solution)/shard_map/ppermute | solution.py:521
  48.3 19.0 %collective-permute-start.19 = (bf16[512,512]{1,0:T(8,128)(2,1)S(1)}, bf16[512,512]{1,0:T(8,128)(2,1)S(1)}, u32[]{:S(2)}, u32[]{:S(2)}) collective-permute-start(bf16[512,512]{1,0:T(8,128)(2,1)S(1)} %attend_1_1_3.1.refs_14_.refs_10_), channel_id=1, source_target_pairs={{0,2},{2,0},{1,3},{3,1},{4,6},{6,4},{5,7},{7,5},{8,10},{10,8},{9,1... | collective-permute-start | bytes 1572872 | tf_op jit(solution)/shard_map/ppermute | solution.py:521
  51.0 11.6 %collective-permute-start.22 = (f32[2,2,128,128]{3,2,1,0:T(8,128)S(1)}, f32[2,2,128,128]{3,2,1,0:T(8,128)S(1)}, u32[]{:S(2)}, u32[]{:S(2)}) collective-permute-start(f32[2,2,128,128]{3,2,1,0:T(8,128)S(1)} %get-tuple-element.53), channel_id=1, source_target_pairs={{0,4},{4,0},{1,5},{5,1},{2,6},{6,2},{3,7},{7,3},{8,12},{12,8},{9,1... | collective-permute-start | bytes 786440 | tf_op jit(solution)/shard_map/ppermute | solution.py:521
  51.6 7.3 %collective-permute-start.20 = (s16[528,128]{1,0:T(8,128)(2,1)S(1)}, s16[528,128]{1,0:T(8,128)(2,1)S(1)}, u32[]{:S(2)}, u32[]{:S(2)}) collective-permute-start(s16[528,128]{1,0:T(8,128)(2,1)S(1)} %get-tuple-element.51), channel_id=1, source_target_pairs={{0,4},{2,6},{4,0},{6,2},{1,5},{3,7},{5,1},{7,3},{8,12},{10,14},{12... | collective-permute-start | bytes 405512 | tf_op jit(solution)/shard_map/ppermute | solution.py:521

commit v11 on v10

--- a/solution.py
+++ b/solution.py
@@ -581,8 +581,8 @@
         after = [own[-1], query[1]]
     levels = []
     for half in halves:
-        level = level_states(plan, own[half], others[half], half, after)
-        levels.append([to_later(level, d) for d in range(plan.n_outer - 1, 0, -1)])
+        level = level_states(plan, own[half], others[half][::-1], half, after)
+        levels.append([to_later(level, d) for d in range(1, plan.n_outer)])
         after = [level]
     local = {}
     for y in range(1, plan.n_y):

time: 68.9 us -> 68.9 us (level)
  waiting for transfers between devices: 11.1 us -> 10.2 us
  starting transfers between devices: 32.6 us -> 33.5 us
    ppermute x17, waiting for transfers between devices: 11.1 us -> 10.2 us  [swap(): return lax.ppermute(array, axes, [(i, i ^ offset) for i in range(size)])]
  transfers between devices with their start and end apart: 23 -> 23, of which waited for: 6 -> 5; matrix products, arithmetic and copies ran while one was open for 0% -> 0% of each run, Pallas kernels for 27% -> 27%
where the time goes in v11:
time: 68.9 us; the launch traced here: 68.7 us
  starting transfers between devices  33.5 us (49%)
  Pallas kernels  24.1 us (35%)
  waiting for transfers between devices  10.2 us (15%)
  between operations  0.87 us (1%)
    ppermute x17, starting transfers between devices, swap(): return lax.ppermute(array, axes, [(i, i ^ offset) for i in range(size)])  20.1 us
    ppermute x6, starting transfers between devices, to_later(): return lax.ppermute(array, 'outer', pairs)  13.4 us
    ppermute x17, waiting for transfers between devices, swap(): return lax.ppermute(array, axes, [(i, i ^ offset) for i in range(size)])  10.2 us
    pallas_call x4, Pallas kernels, attend(): pl.pallas_call(kernel, out_shape=jax.ShapeDtypeStruct((CORES * rows, head...  6.75 us
    pallas_call x1, Pallas kernels, decode(): pl.pallas_call(kernel, out_shape=[jax.ShapeDtypeStruct((rows, plan.n_y *...  4.36 us
    pallas_call x2, Pallas kernels, assemble(): pl.pallas_call(kernel, out_shape=jax.ShapeDtypeStruct((plan.n_y * rows, p...  3.08 us
    pallas_call x2, Pallas kernels, chunk_states(): pl.pallas_call(kernel, out_shape=[states_shape(plan.each), states_shape(p...  2.1 us
    pallas_call x2, Pallas kernels, carries(): pl.pallas_call(kernel, out_shape=[coded_shape(plan.each)] * len(offsets),...  1.5 us
  transfers between devices with their start and end apart: 23, of which 5 were waited for; matrix products, arithmetic and copies ran while one was open for 0% of the time, Pallas kernels for 27%

profile of v11, /device:TPU:0, one launch (start us, length us, event | category | flops | bytes accessed | tf_op | source)
XLA Modules:
  0.0 68.7 jit_solution(3291392868463911942)
XLA Ops:
  0.6 0.1 pad_add_fusion.place_ref
  0.7 4.4 %decode.1 = (bf16[256,2048]{1,0:T(8,128)(2,1)S(1)}, bf16[256,2048]{1,0:T(8,128)(2,1)S(1)}, bf16[256,2048]{1,0:T(8,128)(2,1)S(1)}, bf16[256,2048]{1,0:T(8,128)(2,...) custom-call(s32[4]{0:T(128)S(1)} %pad_add_fusion.place_ref, s32[256,4096]{1,0:T(8,128)} %refs_0_.1, ...), custom_call_target="tpu_custom_call" | custom-call | flops 4194304 | bytes 14680064 | tf_op jit(solution)/shard_map/decode/pallas_call | solution.py:100
  5.1 0.5 collective-permute-start.1
  5.6 0.1 collective-permute-start.2
  5.7 0.8 %spike_queries.1 = (bf16[256,2048]{1,0:T(8,128)(2,1)S(1)}, bf16[256,2048]{1,0:T(8,128)(2,1)S(1)}) custom-call(s32[4]{0:T(128)S(1)} %pad_add_fusion.place_ref, bf16[256,4096]{1,0:T(8,128)(2,1)S(1)} %copy-done, bf16[256,2048]{1,0:T(8,128)(2,1)S(1)} %get-tuple-element.28.refs_0_, bf16[256,2048]{1,0:T(8,128)(2,1)S(1)} %get-tuple-element.29.refs_1_), custom_call_target="tpu_custom_call" | custom-call | flops 1048576 | bytes 6291456 | tf_op jit(solution)/shard_map/spike_queries/pallas_call | solution.py:122
  6.4 0.5 collective-permute-start
  6.9 1.4 %core_states.1.mine_ref = f32[2,4,2,128,128]{4,3,2,1,0:T(8,128)S(1)} custom-call(s32[4]{0:T(128)S(1)} %pad_add_fusion.place_ref, bf16[256,2048]{1,0:T(8,128)(2,1)S(1)} %get-tuple-element.32.k_ref.refs_2_, bf16[256,2048]{1,0:T(8,128)(2,1)S(1)} %get-tuple-element.34.v_ref.refs_4_, bf16[256,2048]{1,0:T(8,128)(2,1)S(1)} %get-tuple-element.30.refs_0_.q_ref), custom_call_target="tpu_custom_call" | custom-call | flops 134217728 | bytes 3145728 | tf_op jit(solution)/shard_map/core_states/pallas_call | solution.py:220
  8.3 0.0 collective-permute-done.1.k_sib_ref.refs_3_
  8.3 1.1 %collective-permute-done.2.v_sib_ref.refs_5_ = bf16[256,2048]{1,0:T(8,128)(2,1)S(1)} collective-permute-done((bf16[256,2048]{1,0:T(8,128)(2,1)S(1)}, bf16[256,2048]{1,0:T(8,128)(2,1)S(1)}, u32[]{:S(2)}, u32[]{:S(2)}) %collective-permute-start.2) | collective-permute-done | bytes 1048608 | tf_op jit(solution)/shard_map/ppermute | solution.py:521
  9.4 1.0 %chunk_states_0.1 = (f32[2,128,128]{2,1,0:T(8,128)S(1)}, f32[4,2,128,128]{3,2,1,0:T(8,128)S(1)}, s16[288,128]{1,0:T(8,128)(2,1)S(1)}, s16[272,128]{1,0:T(8,128)(2,1)S(1)}, s16[272,128]{1,0:T(8,128)(2,1)S(1)}) custom-call(s32[4]{0:T(128)S(1)} %pad_add_fusion.place_ref, f32[2,4,2,128,128]{4,3,2,1,0:T(8,128)S(1)} %core_states.1.mine_ref, ...), custom_call_target="tpu_custom_call" | custom-call | flops 67108864 | bytes 2359296 | tf_op jit(solution)/shard_map/chunk_states_0/pallas_call | solution.py:254
  10.4 2.9 %collective-permute-start.3 = (s16[288,128]{1,0:T(8,128)(2,1)S(1)}, s16[288,128]{1,0:T(8,128)(2,1)S(1)}, u32[]{:S(2)}, u32[]{:S(2)}) collective-permute-start(s16[288,128]{1,0:T(8,128)(2,1)S(1)} %get-tuple-element.38), channel_id=1, source_target_pairs={{0,2},{2,0},{4,6},{6,4},{1,3},{3,1},{5,7},{7,5},{8,10},{10,8},{12,... | collective-permute-start | bytes 221192 | tf_op jit(solution)/shard_map/ppermute | solution.py:521
  13.4 1.4 %collective-permute-start.7 = (s16[272,128]{1,0:T(8,128)(2,1)S(1)}, s16[272,128]{1,0:T(8,128)(2,1)S(1)}, u32[]{:S(2)}, u32[]{:S(2)}) collective-permute-start(s16[272,128]{1,0:T(8,128)(2,1)S(1)} %get-tuple-element.43), channel_id=1, source_target_pairs={{0,6},{2,4},{4,2},{6,0},{1,7},{3,5},{5,3},{7,1},{8,14},{10,12},{12... | collective-permute-start | bytes 208904 | tf_op jit(solution)/shard_map/ppermute | solution.py:521
  14.8 0.1 collective-permute-start.8
  14.9 0.0 collective-permute-done.refs_1_.refs_4_.q_sib_ref
  14.9 1.0 %chunk_states_1.1 = (f32[2,128,128]{2,1,0:T(8,128)S(1)}, f32[4,2,128,128]{3,2,1,0:T(8,128)S(1)}, s16[272,128]{1,0:T(8,128)(2,1)S(1)}, s16[272,128]{1,0:T(8,128)(2,1)S(1)}, s16[272,128]{1,0:T(8,128)(2,1)S(1)}) custom-call(s32[4]{0:T(128)S(1)} %pad_add_fusion.place_ref, f32[2,4,2,128,128]{4,3,2,1,0:T(8,128)S(1)} %core_states.1.mine_ref, ...), custom_call_target="tpu_custom_call" | custom-call | flops 67108864 | bytes 2359296 | tf_op jit(solution)/shard_map/chunk_states_1/pallas_call | solution.py:254
  16.0 2.0 %collective-permute-start.4 = (s16[272,128]{1,0:T(8,128)(2,1)S(1)}, s16[272,128]{1,0:T(8,128)(2,1)S(1)}, u32[]{:S(2)}, u32[]{:S(2)}) collective-permute-start(s16[272,128]{1,0:T(8,128)(2,1)S(1)} %get-tuple-element.40), channel_id=1, source_target_pairs={{0,2},{2,0},{4,6},{6,4},{1,3},{3,1},{5,7},{7,5},{8,10},{10,8},{12,... | collective-permute-start | bytes 208904 | tf_op jit(solution)/shard_map/ppermute | solution.py:521
  18.0 1.5 %collective-permute-start.5 = (s16[272,128]{1,0:T(8,128)(2,1)S(1)}, s16[272,128]{1,0:T(8,128)(2,1)S(1)}, u32[]{:S(2)}, u32[]{:S(2)}) collective-permute-start(s16[272,128]{1,0:T(8,128)(2,1)S(1)} %get-tuple-element.41), channel_id=1, source_target_pairs={{0,4},{2,6},{4,0},{6,2},{1,5},{3,7},{5,1},{7,3},{8,12},{10,14},{12... | collective-permute-start | bytes 208904 | tf_op jit(solution)/shard_map/ppermute | solution.py:521
  19.5 0.0 collective-permute-done.7.refs_0_.refs_2_.refs_3_
  19.5 0.9 %collective-permute-start.6 = (s16[272,128]{1,0:T(8,128)(2,1)S(1)}, s16[272,128]{1,0:T(8,128)(2,1)S(1)}, u32[]{:S(2)}, u32[]{:S(2)}) collective-permute-start(s16[272,128]{1,0:T(8,128)(2,1)S(1)} %get-tuple-element.42), channel_id=1, source_target_pairs={{0,6},{2,4},{4,2},{6,0},{1,7},{3,5},{5,3},{7,1},{8,14},{10,12},{12... | collective-permute-start | bytes 208904 | tf_op jit(solution)/shard_map/ppermute | solution.py:521
  20.4 0.0 collective-permute-done.8.refs_1_.refs_2_
  20.4 0.0 collective-permute-done.3.refs_2_.refs_0_.refs_4_.refs_7_.refs_1_
  20.4 0.1 level_states_0.1.refs_3_
  20.5 5.5 %collective-permute-start.14 = (s16[272,128]{1,0:T(8,128)(2,1)S(1)}, s16[272,128]{1,0:T(8,128)(2,1)S(1)}, u32[]{:S(2)}, u32[]{:S(2)}) collective-permute-start(s16[272,128]{1,0:T(8,128)(2,1)S(1)} %level_states_0.1.refs_3_), channel_id=1, source_target_pairs={{0,24},{1,25},{2,26},{3,27},{4,28},{5,29},{6,30},{7,31}} | collective-permute-start | bytes 208904 | tf_op jit(solution)/shard_map/ppermute | solution.py:528
  26.0 1.3 %collective-permute-start.13 = (s16[272,128]{1,0:T(8,128)(2,1)S(1)}, s16[272,128]{1,0:T(8,128)(2,1)S(1)}, u32[]{:S(2)}, u32[]{:S(2)}) collective-permute-start(s16[272,128]{1,0:T(8,128)(2,1)S(1)} %level_states_0.1.refs_3_), channel_id=1, source_target_pairs={{0,16},{8,24},{1,17},{9,25},{2,18},{10,26},{3,19},{11,27},{4,20},{... | collective-permute-start | bytes 208904 | tf_op jit(solution)/shard_map/ppermute | solution.py:528
  27.4 0.0 collective-permute-done.4.refs_2_.refs_0_.refs_8_
  27.4 2.5 %collective-permute-start.12 = (s16[272,128]{1,0:T(8,128)(2,1)S(1)}, s16[272,128]{1,0:T(8,128)(2,1)S(1)}, u32[]{:S(2)}, u32[]{:S(2)}) collective-permute-start(s16[272,128]{1,0:T(8,128)(2,1)S(1)} %level_states_0.1.refs_3_), channel_id=1, source_target_pairs={{0,8},{8,16},{16,24},{1,9},{9,17},{17,25},{2,10},{10,18},{18,26},{... | collective-permute-start | bytes 208904 | tf_op jit(solution)/shard_map/ppermute | solution.py:528
  29.8 0.0 collective-permute-done.5.refs_1_.refs_9_
  29.9 0.0 collective-permute-done.6.refs_0_.refs_2_.refs_10_
  29.9 0.1 level_states_1.1.refs_0_
  30.0 1.3 %collective-permute-start.11 = (s16[272,128]{1,0:T(8,128)(2,1)S(1)}, s16[272,128]{1,0:T(8,128)(2,1)S(1)}, u32[]{:S(2)}, u32[]{:S(2)}) collective-permute-start(s16[272,128]{1,0:T(8,128)(2,1)S(1)} %level_states_1.1.refs_0_), channel_id=1, source_target_pairs={{0,24},{1,25},{2,26},{3,27},{4,28},{5,29},{6,30},{7,31}} | collective-permute-start | bytes 208904 | tf_op jit(solution)/shard_map/ppermute | solution.py:528
  31.3 1.3 %collective-permute-start.10 = (s16[272,128]{1,0:T(8,128)(2,1)S(1)}, s16[272,128]{1,0:T(8,128)(2,1)S(1)}, u32[]{:S(2)}, u32[]{:S(2)}) collective-permute-start(s16[272,128]{1,0:T(8,128)(2,1)S(1)} %level_states_1.1.refs_0_), channel_id=1, source_target_pairs={{0,16},{8,24},{1,17},{9,25},{2,18},{10,26},{3,19},{11,27},{4,20},{... | collective-permute-start | bytes 208904 | tf_op jit(solution)/shard_map/ppermute | solution.py:528
  32.6 0.0 collective-permute-done.14.refs_5_.refs_6_
  32.6 1.5 %collective-permute-start.9 = (s16[272,128]{1,0:T(8,128)(2,1)S(1)}, s16[272,128]{1,0:T(8,128)(2,1)S(1)}, u32[]{:S(2)}, u32[]{:S(2)}) collective-permute-start(s16[272,128]{1,0:T(8,128)(2,1)S(1)} %level_states_1.1.refs_0_), channel_id=1, source_target_pairs={{0,8},{8,16},{16,24},{1,9},{9,17},{17,25},{2,10},{10,18},{18,26},{... | collective-permute-start | bytes 208904 | tf_op jit(solution)/shard_map/ppermute | solution.py:528
  34.1 1.5 %attend_local_0_1_3.1.refs_6_.refs_2_ = f32[2,256,512]{2,1,0:T(8,128)S(1)} custom-call(s32[4]{0:T(128)S(1)} %pad_add_fusion.place_ref, bf16[256,2048]{1,0:T(8,128)(2,1)S(1)} %get-tuple-element.30.refs_0_.q_ref, bf16[256,2048]{1,0:T(8,128)(2,1)S(1)} %collective-permute-done.refs_1_.refs_4_.q_sib_ref, bf16[256,2048]{1,0:T(8,128)(2,1)S(1)} %get-tuple-element.32.k_ref.refs_2_, ...), custom_call_target="tpu_custom_call" | custom-call | flops 268435456 | bytes 2097152 | tf_op jit(solution)/shard_map/attend_local_0_1_3/pallas_call | solution.py:374
  35.6 0.0 collective-permute-done.13.refs_4_.refs_5_
  35.6 0.0 collective-permute-done.12.refs_3_.refs_4_
  35.6 0.8 %carries_0.1 = (s16[272,128]{1,0:T(8,128)(2,1)S(1)}, s16[272,128]{1,0:T(8,128)(2,1)S(1)}) custom-call(s32[4]{0:T(128)S(1)} %pad_add_fusion.place_ref, f32[2,128,128]{2,1,0:T(8,128)S(1)} %get-tuple-element.36.refs_0_.own_ref, s16[288,128]{1,0:T(8,128)(2,1)S(1)} %collective-permute-done.3.refs_2_.refs_0_.refs_4_.refs_7_.refs_1_, ...), custom_call_target="tpu_custom_call" | custom-call | bytes 1245184 | tf_op jit(solution)/shard_map/carries_0/pallas_call | solution.py:316
  36.4 1.8 %collective-permute-start.18 = (s16[272,128]{1,0:T(8,128)(2,1)S(1)}, s16[272,128]{1,0:T(8,128)(2,1)S(1)}, u32[]{:S(2)}, u32[]{:S(2)}) collective-permute-start(s16[272,128]{1,0:T(8,128)(2,1)S(1)} %get-tuple-element.49), channel_id=1, source_target_pairs={{0,6},{2,4},{4,2},{6,0},{1,7},{3,5},{5,3},{7,1},{8,14},{10,12},{12... | collective-permute-start | bytes 208904 | tf_op jit(solution)/shard_map/ppermute | solution.py:521
  38.2 0.8 %collective-permute-start.17 = (s16[272,128]{1,0:T(8,128)(2,1)S(1)}, s16[272,128]{1,0:T(8,128)(2,1)S(1)}, u32[]{:S(2)}, u32[]{:S(2)}) collective-permute-start(s16[272,128]{1,0:T(8,128)(2,1)S(1)} %get-tuple-element.45.refs_6_), channel_id=1, source_target_pairs={{0,2},{2,0},{4,6},{6,4},{1,3},{3,1},{5,7},{7,5},{8,10},{10,8},{12,... | collective-permute-start | bytes 208904 | tf_op jit(solution)/shard_map/ppermute | solution.py:521
  39.0 0.0 collective-permute-done.11.refs_5_.refs_13_
  39.0 0.0 collective-permute-done.10.refs_4_.refs_12_
  39.0 0.8 %carries_1.1 = (s16[272,128]{1,0:T(8,128)(2,1)S(1)}, s16[272,128]{1,0:T(8,128)(2,1)S(1)}) custom-call(s32[4]{0:T(128)S(1)} %pad_add_fusion.place_ref, f32[2,128,128]{2,1,0:T(8,128)S(1)} %get-tuple-element.39.refs_3_.own_ref.refs_7_, s16[272,128]{1,0:T(8,128)(2,1)S(1)} %collective-permute-done.4.refs_2_.refs_0_.refs_8_, ...), custom_call_target="tpu_custom_call" | custom-call | bytes 1245184 | tf_op jit(solution)/shard_map/carries_1/pallas_call | solution.py:316
  39.8 1.8 %collective-permute-start.16 = (s16[272,128]{1,0:T(8,128)(2,1)S(1)}, s16[272,128]{1,0:T(8,128)(2,1)S(1)}, u32[]{:S(2)}, u32[]{:S(2)}) collective-permute-start(s16[272,128]{1,0:T(8,128)(2,1)S(1)} %get-tuple-element.47), channel_id=1, source_target_pairs={{0,6},{2,4},{4,2},{6,0},{1,7},{3,5},{5,3},{7,1},{8,14},{10,12},{12... | collective-permute-start | bytes 208904 | tf_op jit(solution)/shard_map/ppermute | solution.py:521
  41.6 0.6 collective-permute-start.15
  42.2 0.0 collective-permute-done.18.refs_6_
  42.2 1.2 %collective-permute-done.17.refs_5_ = s16[272,128]{1,0:T(8,128)(2,1)S(1)} collective-permute-done((s16[272,128]{1,0:T(8,128)(2,1)S(1)}, s16[272,128]{1,0:T(8,128)(2,1)S(1)}, u32[]{:S(2)}, u32[]{:S(2)}) %collective-permute-start.17) | collective-permute-done | bytes 69664 | tf_op jit(solution)/shard_map/ppermute | solution.py:521
  43.5 1.2 %attend_0_1_3.1.refs_10_ = bf16[512,512]{1,0:T(8,128)(2,1)S(1)} custom-call(s32[4]{0:T(128)S(1)} %pad_add_fusion.place_ref, bf16[256,2048]{1,0:T(8,128)(2,1)S(1)} %get-tuple-element.30.refs_0_.q_ref, bf16[256,2048]{1,0:T(8,128)(2,1)S(1)} %collective-permute-done.refs_1_.refs_4_.q_sib_ref, f32[2,256,512]{2,1,0:T(8,128)S(1)} %attend_local_0_1_3.1.refs_6_.refs_2_, ...), custom_call_target="tpu_custom_call" | custom-call | flops 402653184 | bytes 2097152 | tf_op jit(solution)/shard_map/attend_0_1_3/pallas_call | solution.py:446
  44.6 1.6 %collective-permute-start.21 = (bf16[512,512]{1,0:T(8,128)(2,1)S(1)}, bf16[512,512]{1,0:T(8,128)(2,1)S(1)}, u32[]{:S(2)}, u32[]{:S(2)}) collective-permute-start(bf16[512,512]{1,0:T(8,128)(2,1)S(1)} %attend_0_1_3.1.refs_10_), channel_id=1, source_target_pairs={{0,2},{2,0},{1,3},{3,1},{4,6},{6,4},{5,7},{7,5},{8,10},{10,8},{9,1... | collective-permute-start | bytes 1572872 | tf_op jit(solution)/shard_map/ppermute | solution.py:521
  46.2 0.0 collective-permute-done.16.refs_9_
  46.2 0.5 collective-permute-done.15.refs_8_
  46.7 1.9 %attend_1_1_3.1.refs_14_.refs_10_ = bf16[512,512]{1,0:T(8,128)(2,1)S(1)} custom-call(s32[4]{0:T(128)S(1)} %pad_add_fusion.place_ref, bf16[256,2048]{1,0:T(8,128)(2,1)S(1)} %get-tuple-element.30.refs_0_.q_ref, bf16[256,2048]{1,0:T(8,128)(2,1)S(1)} %collective-permute-done.refs_1_.refs_4_.q_sib_ref, bf16[256,2048]{1,0:T(8,128)(2,1)S(1)} %get-tuple-element.32.k_ref.refs_2_, ...), custom_call_target="tpu_custom_call" | custom-call | flops 402653184 | bytes 2097152 | tf_op jit(solution)/shard_map/attend_1_1_3/pallas_call | solution.py:446
  48.6 1.3 %collective-permute-start.19 = (bf16[512,512]{1,0:T(8,128)(2,1)S(1)}, bf16[512,512]{1,0:T(8,128)(2,1)S(1)}, u32[]{:S(2)}, u32[]{:S(2)}) collective-permute-start(bf16[512,512]{1,0:T(8,128)(2,1)S(1)} %attend_1_1_3.1.refs_14_.refs_10_), channel_id=1, source_target_pairs={{0,2},{2,0},{1,3},{3,1},{4,6},{6,4},{5,7},{7,5},{8,10},{10,8},{9,1... | collective-permute-start | bytes 1572872 | tf_op jit(solution)/shard_map/ppermute | solution.py:521
  49.9 1.1 %own_carries.1 = (s16[528,128]{1,0:T(8,128)(2,1)S(1)}, s16[528,128]{1,0:T(8,128)(2,1)S(1)}, f32[2,2,128,128]{3,2,1,0:T(8,128)S(1)}, f32[2,2,128,128]{3,2,1,0:T(8,128)S(1)}) custom-call(s32[4]{0:T(128)S(1)} %pad_add_fusion.place_ref, f32[2,128,128]{2,1,0:T(8,128)S(1)} %get-tuple-element.36.refs_0_.own_ref, ...), custom_call_target="tpu_custom_call" | custom-call | bytes 2621440 | tf_op jit(solution)/shard_map/own_carries/pallas_call | solution.py:350
  51.0 1.1 %collective-permute-start.22 = (f32[2,2,128,128]{3,2,1,0:T(8,128)S(1)}, f32[2,2,128,128]{3,2,1,0:T(8,128)S(1)}, u32[]{:S(2)}, u32[]{:S(2)}) collective-permute-start(f32[2,2,128,128]{3,2,1,0:T(8,128)S(1)} %get-tuple-element.53), channel_id=1, source_target_pairs={{0,4},{4,0},{1,5},{5,1},{2,6},{6,2},{3,7},{7,3},{8,12},{12,8},{9,1... | collective-permute-start | bytes 786440 | tf_op jit(solution)/shard_map/ppermute | solution.py:521
  52.1 1.0 %collective-permute-start.20 = (s16[528,128]{1,0:T(8,128)(2,1)S(1)}, s16[528,128]{1,0:T(8,128)(2,1)S(1)}, u32[]{:S(2)}, u32[]{:S(2)}) collective-permute-start(s16[528,128]{1,0:T(8,128)(2,1)S(1)} %get-tuple-element.51), channel_id=1, source_target_pairs={{0,4},{2,6},{4,0},{6,2},{1,5},{3,7},{5,1},{7,3},{8,12},{10,14},{12... | collective-permute-start | bytes 405512 | tf_op jit(solution)/shard_map/ppermute | solution.py:521
  53.1 5.8 %collective-permute-done.20.refs_9_ = s16[528,128]{1,0:T(8,128)(2,1)S(1)} collective-permute-done((s16[528,128]{1,0:T(8,128)(2,1)S(1)}, s16[528,128]{1,0:T(8,128)(2,1)S(1)}, u32[]{:S(2)}, u32[]{:S(2)}) %collective-permute-start.20) | collective-permute-done | bytes 135200 | tf_op jit(solution)/shard_map/ppermute | solution.py:521
  58.9 1.9 %attend_0_0_2.1.refs_10_.refs_0_ = bf16[512,512]{1,0:T(8,128)(2,1)S(1)} custom-call(s32[4]{0:T(128)S(1)} %pad_add_fusion.place_ref, bf16[256,2048]{1,0:T(8,128)(2,1)S(1)} %get-tuple-element.30.refs_0_.q_ref, bf16[256,2048]{1,0:T(8,128)(2,1)S(1)} %collective-permute-done.refs_1_.refs_4_.q_sib_ref, bf16[256,2048]{1,0:T(8,128)(2,1)S(1)} %get-tuple-element.32.k_ref.refs_2_, ...), custom_call_target="tpu_custom_call" | custom-call | flops 402653184 | bytes 2097152 | tf_op jit(solution)/shard_map/attend_0_0_2/pallas_call | solution.py:446
  60.7 1.9 %attend_1_0_2.1.refs_1_ = bf16[512,512]{1,0:T(8,128)(2,1)S(1)} custom-call(s32[4]{0:T(128)S(1)} %pad_add_fusion.place_ref, bf16[256,2048]{1,0:T(8,128)(2,1)S(1)} %get-tuple-element.30.refs_0_.q_ref, bf16[256,2048]{1,0:T(8,128)(2,1)S(1)} %collective-permute-done.refs_1_.refs_4_.q_sib_ref, bf16[256,2048]{1,0:T(8,128)(2,1)S(1)} %get-tuple-element.32.k_ref.refs_2_, ...), custom_call_target="tpu_custom_call" | custom-call | flops 402653184 | bytes 2097152 | tf_op jit(solution)/shard_map/attend_1_0_2/pallas_call | solution.py:446
  62.6 0.0 collective-permute-done.22.refs_1_
  62.6 1.4 %assemble_cache.1 = f32[1,8,128,128]{3,2,1,0:T(8,128)} custom-call(s32[4]{0:T(128)S(1)} %pad_add_fusion.place_ref, f32[2,2,128,128]{3,2,1,0:T(8,128)S(1)} %get-tuple-element.52.refs_0_, f32[2,2,128,128]{3,2,1,0:T(8,128)S(1)} %collective-permute-done.22.refs_1_), custom_call_target="tpu_custom_call" | custom-call | tf_op jit(solution)/shard_map/assemble_cache/pallas_call | solution.py:506
  64.0 0.0 collective-permute-done.21.refs_2_
  64.0 1.7 %assemble.1.refs_1_ = bf16[1024,1024]{1,0:T(8,128)(2,1)} custom-call(s32[4]{0:T(128)S(1)} %pad_add_fusion.place_ref, bf16[512,512]{1,0:T(8,128)(2,1)S(1)} %attend_0_0_2.1.refs_10_.refs_0_, bf16[512,512]{1,0:T(8,128)(2,1)S(1)} %attend_1_0_2.1.refs_1_, bf16[512,512]{1,0:T(8,128)(2,1)S(1)} %collective-permute-done.21.refs_2_), custom_call_target="tpu_custom_call" | custom-call | tf_op jit(solution)/shard_map/assemble/pallas_call | solution.py:485
  65.7 1.6 %collective-permute-done.19.refs_0_ = bf16[512,512]{1,0:T(8,128)(2,1)S(1)} collective-permute-done((bf16[512,512]{1,0:T(8,128)(2,1)S(1)}, bf16[512,512]{1,0:T(8,128)(2,1)S(1)}, u32[]{:S(2)}, u32[]{:S(2)}) %collective-permute-start.19) | collective-permute-done | bytes 524320 | tf_op jit(solution)/shard_map/ppermute | solution.py:521
  67.3 1.4 %finish.1 = bf16[1024,1024]{1,0:T(8,128)(2,1)} custom-call(s32[4]{0:T(128)S(1)} %pad_add_fusion.place_ref, bf16[512,512]{1,0:T(8,128)(2,1)S(1)} %collective-permute-done.19.refs_0_, bf16[1024,1024]{1,0:T(8,128)(2,1)} %assemble.1.refs_1_), custom_call_target="tpu_custom_call", output_to_operand_aliasing={{}: (2, {})} | custom-call | tf_op jit(solution)/shard_map/finish/pallas_call | solution.py:485
  (5 shorter events, 0.0 us)
Async XLA Ops:
  0.7 5.0 %copy-start = (bf16[256,4096]{1,0:T(8,128)(2,1)S(1)}, bf16[256,4096]{1,0:T(8,128)(2,1)}, u32[]{:S(2)}) copy-start(bf16[256,4096]{1,0:T(8,128)(2,1)} %queries_ref.1) | copy-start | bytes 6291460
  5.1 3.2 %collective-permute-start.1 = (bf16[256,2048]{1,0:T(8,128)(2,1)S(1)}, bf16[256,2048]{1,0:T(8,128)(2,1)S(1)}, u32[]{:S(2)}, u32[]{:S(2)}) collective-permute-start(bf16[256,2048]{1,0:T(8,128)(2,1)S(1)} %get-tuple-element.33), channel_id=1, source_target_pairs={{0,1},{1,0},{2,3},{3,2},{4,5},{5,4},{6,7},{7,6},{8,9},{9,8},{10,11... | collective-permute-start | bytes 3145736 | tf_op jit(solution)/shard_map/ppermute | solution.py:521
  5.6 3.8 %collective-permute-start.2 = (bf16[256,2048]{1,0:T(8,128)(2,1)S(1)}, bf16[256,2048]{1,0:T(8,128)(2,1)S(1)}, u32[]{:S(2)}, u32[]{:S(2)}) collective-permute-start(bf16[256,2048]{1,0:T(8,128)(2,1)S(1)} %get-tuple-element.35), channel_id=1, source_target_pairs={{0,1},{1,0},{2,3},{3,2},{4,5},{5,4},{6,7},{7,6},{8,9},{9,8},{10,11... | collective-permute-start | bytes 3145736 | tf_op jit(solution)/shard_map/ppermute | solution.py:521
  6.4 8.5 %collective-permute-start = (bf16[256,2048]{1,0:T(8,128)(2,1)S(1)}, bf16[256,2048]{1,0:T(8,128)(2,1)S(1)}, u32[]{:S(2)}, u32[]{:S(2)}) collective-permute-start(bf16[256,2048]{1,0:T(8,128)(2,1)S(1)} %get-tuple-element.31), channel_id=1, source_target_pairs={{0,1},{1,0},{2,3},{3,2},{4,5},{5,4},{6,7},{7,6},{8,9},{9,8},{10,11... | collective-permute-start | bytes 3145736 | tf_op jit(solution)/shard_map/ppermute | solution.py:521
  6.9 2.5 %copy-start.1 = (f32[1024]{0:T(1024)S(1)}, f32[1024]{0:T(1024)}, u32[]{:S(2)}) copy-start(f32[1024]{0:T(1024)} %param.9) | copy-start | bytes 12292
  10.4 10.0 %collective-permute-start.3 = (s16[288,128]{1,0:T(8,128)(2,1)S(1)}, s16[288,128]{1,0:T(8,128)(2,1)S(1)}, u32[]{:S(2)}, u32[]{:S(2)}) collective-permute-start(s16[288,128]{1,0:T(8,128)(2,1)S(1)} %get-tuple-element.38), channel_id=1, source_target_pairs={{0,2},{2,0},{4,6},{6,4},{1,3},{3,1},{5,7},{7,5},{8,10},{10,8},{12,... | collective-permute-start | bytes 221192 | tf_op jit(solution)/shard_map/ppermute | solution.py:521
  13.4 6.1 %collective-permute-start.7 = (s16[272,128]{1,0:T(8,128)(2,1)S(1)}, s16[272,128]{1,0:T(8,128)(2,1)S(1)}, u32[]{:S(2)}, u32[]{:S(2)}) collective-permute-start(s16[272,128]{1,0:T(8,128)(2,1)S(1)} %get-tuple-element.43), channel_id=1, source_target_pairs={{0,6},{2,4},{4,2},{6,0},{1,7},{3,5},{5,3},{7,1},{8,14},{10,12},{12... | collective-permute-start | bytes 208904 | tf_op jit(solution)/shard_map/ppermute | solution.py:521
  14.8 5.6 %collective-permute-start.8 = (s16[272,128]{1,0:T(8,128)(2,1)S(1)}, s16[272,128]{1,0:T(8,128)(2,1)S(1)}, u32[]{:S(2)}, u32[]{:S(2)}) collective-permute-start(s16[272,128]{1,0:T(8,128)(2,1)S(1)} %get-tuple-element.44), channel_id=1, source_target_pairs={{0,4},{2,6},{4,0},{6,2},{1,5},{3,7},{5,1},{7,3},{8,12},{10,14},{12... | collective-permute-start | bytes 208904 | tf_op jit(solution)/shard_map/ppermute | solution.py:521
  16.0 11.4 %collective-permute-start.4 = (s16[272,128]{1,0:T(8,128)(2,1)S(1)}, s16[272,128]{1,0:T(8,128)(2,1)S(1)}, u32[]{:S(2)}, u32[]{:S(2)}) collective-permute-start(s16[272,128]{1,0:T(8,128)(2,1)S(1)} %get-tuple-element.40), channel_id=1, source_target_pairs={{0,2},{2,0},{4,6},{6,4},{1,3},{3,1},{5,7},{7,5},{8,10},{10,8},{12,... | collective-permute-start | bytes 208904 | tf_op jit(solution)/shard_map/ppermute | solution.py:521
  18.0 11.8 %collective-permute-start.5 = (s16[272,128]{1,0:T(8,128)(2,1)S(1)}, s16[272,128]{1,0:T(8,128)(2,1)S(1)}, u32[]{:S(2)}, u32[]{:S(2)}) collective-permute-start(s16[272,128]{1,0:T(8,128)(2,1)S(1)} %get-tuple-element.41), channel_id=1, source_target_pairs={{0,4},{2,6},{4,0},{6,2},{1,5},{3,7},{5,1},{7,3},{8,12},{10,14},{12... | collective-permute-start | bytes 208904 | tf_op jit(solution)/shard_map/ppermute | solution.py:521
  19.5 10.3 %collective-permute-start.6 = (s16[272,128]{1,0:T(8,128)(2,1)S(1)}, s16[272,128]{1,0:T(8,128)(2,1)S(1)}, u32[]{:S(2)}, u32[]{:S(2)}) collective-permute-start(s16[272,128]{1,0:T(8,128)(2,1)S(1)} %get-tuple-element.42), channel_id=1, source_target_pairs={{0,6},{2,4},{4,2},{6,0},{1,7},{3,5},{5,3},{7,1},{8,14},{10,12},{12... | collective-permute-start | bytes 208904 | tf_op jit(solution)/shard_map/ppermute | solution.py:521
  20.5 12.0 %collective-permute-start.14 = (s16[272,128]{1,0:T(8,128)(2,1)S(1)}, s16[272,128]{1,0:T(8,128)(2,1)S(1)}, u32[]{:S(2)}, u32[]{:S(2)}) collective-permute-start(s16[272,128]{1,0:T(8,128)(2,1)S(1)} %level_states_0.1.refs_3_), channel_id=1, source_target_pairs={{0,24},{1,25},{2,26},{3,27},{4,28},{5,29},{6,30},{7,31}} | collective-permute-start | bytes 208904 | tf_op jit(solution)/shard_map/ppermute | solution.py:528
  26.0 9.6 %collective-permute-start.13 = (s16[272,128]{1,0:T(8,128)(2,1)S(1)}, s16[272,128]{1,0:T(8,128)(2,1)S(1)}, u32[]{:S(2)}, u32[]{:S(2)}) collective-permute-start(s16[272,128]{1,0:T(8,128)(2,1)S(1)} %level_states_0.1.refs_3_), channel_id=1, source_target_pairs={{0,16},{8,24},{1,17},{9,25},{2,18},{10,26},{3,19},{11,27},{4,20},{... | collective-permute-start | bytes 208904 | tf_op jit(solution)/shard_map/ppermute | solution.py:528
  27.4 8.3 %collective-permute-start.12 = (s16[272,128]{1,0:T(8,128)(2,1)S(1)}, s16[272,128]{1,0:T(8,128)(2,1)S(1)}, u32[]{:S(2)}, u32[]{:S(2)}) collective-permute-start(s16[272,128]{1,0:T(8,128)(2,1)S(1)} %level_states_0.1.refs_3_), channel_id=1, source_target_pairs={{0,8},{8,16},{16,24},{1,9},{9,17},{17,25},{2,10},{10,18},{18,26},{... | collective-permute-start | bytes 208904 | tf_op jit(solution)/shard_map/ppermute | solution.py:528
  30.0 9.0 %collective-permute-start.11 = (s16[272,128]{1,0:T(8,128)(2,1)S(1)}, s16[272,128]{1,0:T(8,128)(2,1)S(1)}, u32[]{:S(2)}, u32[]{:S(2)}) collective-permute-start(s16[272,128]{1,0:T(8,128)(2,1)S(1)} %level_states_1.1.refs_0_), channel_id=1, source_target_pairs={{0,24},{1,25},{2,26},{3,27},{4,28},{5,29},{6,30},{7,31}} | collective-permute-start | bytes 208904 | tf_op jit(solution)/shard_map/ppermute | solution.py:528
  31.3 7.7 %collective-permute-start.10 = (s16[272,128]{1,0:T(8,128)(2,1)S(1)}, s16[272,128]{1,0:T(8,128)(2,1)S(1)}, u32[]{:S(2)}, u32[]{:S(2)}) collective-permute-start(s16[272,128]{1,0:T(8,128)(2,1)S(1)} %level_states_1.1.refs_0_), channel_id=1, source_target_pairs={{0,16},{8,24},{1,17},{9,25},{2,18},{10,26},{3,19},{11,27},{4,20},{... | collective-permute-start | bytes 208904 | tf_op jit(solution)/shard_map/ppermute | solution.py:528
  32.6 6.4 %collective-permute-start.9 = (s16[272,128]{1,0:T(8,128)(2,1)S(1)}, s16[272,128]{1,0:T(8,128)(2,1)S(1)}, u32[]{:S(2)}, u32[]{:S(2)}) collective-permute-start(s16[272,128]{1,0:T(8,128)(2,1)S(1)} %level_states_1.1.refs_0_), channel_id=1, source_target_pairs={{0,8},{8,16},{16,24},{1,9},{9,17},{17,25},{2,10},{10,18},{18,26},{... | collective-permute-start | bytes 208904 | tf_op jit(solution)/shard_map/ppermute | solution.py:528
  36.4 5.9 %collective-permute-start.18 = (s16[272,128]{1,0:T(8,128)(2,1)S(1)}, s16[272,128]{1,0:T(8,128)(2,1)S(1)}, u32[]{:S(2)}, u32[]{:S(2)}) collective-permute-start(s16[272,128]{1,0:T(8,128)(2,1)S(1)} %get-tuple-element.49), channel_id=1, source_target_pairs={{0,6},{2,4},{4,2},{6,0},{1,7},{3,5},{5,3},{7,1},{8,14},{10,12},{12... | collective-permute-start | bytes 208904 | tf_op jit(solution)/shard_map/ppermute | solution.py:521
  38.2 5.2 %collective-permute-start.17 = (s16[272,128]{1,0:T(8,128)(2,1)S(1)}, s16[272,128]{1,0:T(8,128)(2,1)S(1)}, u32[]{:S(2)}, u32[]{:S(2)}) collective-permute-start(s16[272,128]{1,0:T(8,128)(2,1)S(1)} %get-tuple-element.45.refs_6_), channel_id=1, source_target_pairs={{0,2},{2,0},{4,6},{6,4},{1,3},{3,1},{5,7},{7,5},{8,10},{10,8},{12,... | collective-permute-start | bytes 208904 | tf_op jit(solution)/shard_map/ppermute | solution.py:521
  39.8 6.5 %collective-permute-start.16 = (s16[272,128]{1,0:T(8,128)(2,1)S(1)}, s16[272,128]{1,0:T(8,128)(2,1)S(1)}, u32[]{:S(2)}, u32[]{:S(2)}) collective-permute-start(s16[272,128]{1,0:T(8,128)(2,1)S(1)} %get-tuple-element.47), channel_id=1, source_target_pairs={{0,6},{2,4},{4,2},{6,0},{1,7},{3,5},{5,3},{7,1},{8,14},{10,12},{12... | collective-permute-start | bytes 208904 | tf_op jit(solution)/shard_map/ppermute | solution.py:521
  41.6 5.1 %collective-permute-start.15 = (s16[272,128]{1,0:T(8,128)(2,1)S(1)}, s16[272,128]{1,0:T(8,128)(2,1)S(1)}, u32[]{:S(2)}, u32[]{:S(2)}) collective-permute-start(s16[272,128]{1,0:T(8,128)(2,1)S(1)} %get-tuple-element.46.refs_7_), channel_id=1, source_target_pairs={{0,2},{2,0},{4,6},{6,4},{1,3},{3,1},{5,7},{7,5},{8,10},{10,8},{12,... | collective-permute-start | bytes 208904 | tf_op jit(solution)/shard_map/ppermute | solution.py:521
  44.6 19.4 %collective-permute-start.21 = (bf16[512,512]{1,0:T(8,128)(2,1)S(1)}, bf16[512,512]{1,0:T(8,128)(2,1)S(1)}, u32[]{:S(2)}, u32[]{:S(2)}) collective-permute-start(bf16[512,512]{1,0:T(8,128)(2,1)S(1)} %attend_0_1_3.1.refs_10_), channel_id=1, source_target_pairs={{0,2},{2,0},{1,3},{3,1},{4,6},{6,4},{5,7},{7,5},{8,10},{10,8},{9,1... | collective-permute-start | bytes 1572872 | tf_op jit(solution)/shard_map/ppermute | solution.py:521
  48.6 18.8 %collective-permute-start.19 = (bf16[512,512]{1,0:T(8,128)(2,1)S(1)}, bf16[512,512]{1,0:T(8,128)(2,1)S(1)}, u32[]{:S(2)}, u32[]{:S(2)}) collective-permute-start(bf16[512,512]{1,0:T(8,128)(2,1)S(1)} %attend_1_1_3.1.refs_14_.refs_10_), channel_id=1, source_target_pairs={{0,2},{2,0},{1,3},{3,1},{4,6},{6,4},{5,7},{7,5},{8,10},{10,8},{9,1... | collective-permute-start | bytes 1572872 | tf_op jit(solution)/shard_map/ppermute | solution.py:521
  51.0 11.6 %collective-permute-start.22 = (f32[2,2,128,128]{3,2,1,0:T(8,128)S(1)}, f32[2,2,128,128]{3,2,1,0:T(8,128)S(1)}, u32[]{:S(2)}, u32[]{:S(2)}) collective-permute-start(f32[2,2,128,128]{3,2,1,0:T(8,128)S(1)} %get-tuple-element.53), channel_id=1, source_target_pairs={{0,4},{4,0},{1,5},{5,1},{2,6},{6,2},{3,7},{7,3},{8,12},{12,8},{9,1... | collective-permute-start | bytes 786440 | tf_op jit(solution)/shard_map/ppermute | solution.py:521
  52.1 6.7 %collective-permute-start.20 = (s16[528,128]{1,0:T(8,128)(2,1)S(1)}, s16[528,128]{1,0:T(8,128)(2,1)S(1)}, u32[]{:S(2)}, u32[]{:S(2)}) collective-permute-start(s16[528,128]{1,0:T(8,128)(2,1)S(1)} %get-tuple-element.51), channel_id=1, source_target_pairs={{0,4},{2,6},{4,0},{6,2},{1,5},{3,7},{5,1},{7,3},{8,12},{10,14},{12... | collective-permute-start | bytes 405512 | tf_op jit(solution)/shard_map/ppermute | solution.py:521

commit v12 on v11

--- a/solution.py
+++ b/solution.py
@@ -270,17 +270,35 @@
 
 def level_states(plan, own, others, half, after):
     def kernel(own_ref, *refs):
-        code(total_of((own_ref, *refs[: len(others)]), plan.each), refs[-1])
-
-    return pl.pallas_call(
-        kernel,
-        out_shape=coded_shape(plan.each),
+        total = total_of((own_ref, *refs[: len(others)]), plan.each)
+        for i, state in enumerate(total):
+            refs[-2][i] = state
+        code(total, refs[-1])
+
+    return pl.pallas_call(
+        kernel,
+        out_shape=[states_shape(plan.each), coded_shape(plan.each)],
         in_specs=[VMEM] * plan.plane + [ANY] * len(after),
-        out_specs=VMEM,
+        out_specs=[VMEM] * 2,
         compiler_params=params(),
         cost_estimate=cost(0, plan.plane * plan.each * HD * HD * 2),
         name=f"level_states_{half}",
     )(own, *others, *after)
+
+
+def two_levels(plan, total, before, half, after):
+    def kernel(total_ref, before_ref, *refs):
+        code(total_of((total_ref, before_ref), plan.each), refs[-1])
+
+    return pl.pallas_call(
+        kernel,
+        out_shape=coded_shape(plan.each),
+        in_specs=[VMEM] * 2 + [ANY] * len(after),
+        out_specs=VMEM,
+        compiler_params=params(),
+        cost_estimate=cost(0, 2 * plan.each * HD * HD * 2),
+        name=f"two_levels_{half}",
+    )(total, before, *after)
 
 
 def carried(plan, place_ref, own, others, levels, offsets):
@@ -523,9 +541,11 @@
     def in_level(array, offset):
         return swap(array, ("inner", "y"), offset, plan.plane)
 
-    def to_later(array, distance):
-        pairs = [(i, i + distance) for i in range(plan.n_outer - distance)]
+    def to_later(array, pairs):
         return lax.ppermute(array, "outer", pairs)
+
+    def ahead(distance):
+        return [(i, i + distance) for i in range(plan.n_outer - distance)]
 
     gain = gain.reshape(1, plan.width)
     key, key_out, value, value_out, *counts = decode(plan, place, spikes, keys, values)
@@ -579,11 +599,20 @@
     for half in halves:
         owner_stage(half, after)
         after = [own[-1], query[1]]
-    levels = []
+    levels, totals = [], []
     for half in halves:
-        level = level_states(plan, own[half], others[half][::-1], half, after)
-        levels.append([to_later(level, d) for d in range(1, plan.n_outer)])
+        total, level = level_states(plan, own[half], others[half][::-1], half, after)
+        totals.append(total)
+        if plan.n_outer == 4:
+            levels.append([to_later(level, ahead(1)), to_later(level, [(0, 2)])])
+        else:
+            levels.append([to_later(level, ahead(d)) for d in range(1, plan.n_outer)])
         after = [level]
+    if plan.n_outer == 4:
+        for half in halves:
+            level = two_levels(plan, totals[half], levels[half][0], half, after)
+            levels[half].append(to_later(level, [(1, 3)]))
+            after = [level]
     local = {}
     for y in range(1, plan.n_y):
         local[y] = attend_local(plan, place, query, key, value, 0, of_group[y], after)

time: 68.9 us -> 69.6 us (1.010)
  no operation moved by 1% of the time
where the time goes in v12:
time: 69.6 us; the launch traced here: 69.3 us
  starting transfers between devices  33.8 us (49%)
  Pallas kernels  24.2 us (35%)
  waiting for transfers between devices  10.4 us (15%)
  between operations  0.88 us (1%)
    ppermute x17, starting transfers between devices, swap(): return lax.ppermute(array, axes, [(i, i ^ offset) for i in range(size)])  19.7 us
    ppermute x6, starting transfers between devices, to_later(): return lax.ppermute(array, 'outer', pairs)  14.1 us
    ppermute x17, waiting for transfers between devices, swap(): return lax.ppermute(array, axes, [(i, i ^ offset) for i in range(size)])  10.4 us
    pallas_call x4, Pallas kernels, attend(): pl.pallas_call(kernel, out_shape=jax.ShapeDtypeStruct((CORES * rows, head...  6.75 us
    pallas_call x1, Pallas kernels, decode(): pl.pallas_call(kernel, out_shape=[jax.ShapeDtypeStruct((rows, plan.n_y *...  4.36 us
    pallas_call x2, Pallas kernels, assemble(): pl.pallas_call(kernel, out_shape=jax.ShapeDtypeStruct((plan.n_y * rows, p...  3.08 us
    pallas_call x2, Pallas kernels, chunk_states(): pl.pallas_call(kernel, out_shape=[states_shape(plan.each), states_shape(p...  2.1 us
    pallas_call x2, Pallas kernels, carries(): pl.pallas_call(kernel, out_shape=[coded_shape(plan.each)] * len(offsets),...  1.5 us
  transfers between devices with their start and end apart: 23, of which 5 were waited for; matrix products, arithmetic and copies ran while one was open for 0% of the time, Pallas kernels for 27%

profile of v12, /device:TPU:0, one launch (start us, length us, event | category | flops | bytes accessed | tf_op | source)
XLA Modules:
  0.0 69.3 jit_solution(4213103281731488946)
XLA Ops:
  0.6 0.1 pad_add_fusion.place_ref
  0.7 4.4 %decode.1 = (bf16[256,2048]{1,0:T(8,128)(2,1)S(1)}, bf16[256,2048]{1,0:T(8,128)(2,1)S(1)}, bf16[256,2048]{1,0:T(8,128)(2,1)S(1)}, bf16[256,2048]{1,0:T(8,128)(2,...) custom-call(s32[4]{0:T(128)S(1)} %pad_add_fusion.place_ref, s32[256,4096]{1,0:T(8,128)} %refs_0_.1, ...), custom_call_target="tpu_custom_call" | custom-call | flops 4194304 | bytes 14680064 | tf_op jit(solution)/shard_map/decode/pallas_call | solution.py:100
  5.1 0.5 collective-permute-start.1
  5.6 0.1 collective-permute-start.2
  5.7 0.8 %spike_queries.1 = (bf16[256,2048]{1,0:T(8,128)(2,1)S(1)}, bf16[256,2048]{1,0:T(8,128)(2,1)S(1)}) custom-call(s32[4]{0:T(128)S(1)} %pad_add_fusion.place_ref, bf16[256,4096]{1,0:T(8,128)(2,1)S(1)} %copy-done, bf16[256,2048]{1,0:T(8,128)(2,1)S(1)} %get-tuple-element.32.refs_0_, bf16[256,2048]{1,0:T(8,128)(2,1)S(1)} %get-tuple-element.33.refs_1_), custom_call_target="tpu_custom_call" | custom-call | flops 1048576 | bytes 6291456 | tf_op jit(solution)/shard_map/spike_queries/pallas_call | solution.py:122
  6.4 0.5 collective-permute-start
  6.9 1.4 %core_states.1.mine_ref = f32[2,4,2,128,128]{4,3,2,1,0:T(8,128)S(1)} custom-call(s32[4]{0:T(128)S(1)} %pad_add_fusion.place_ref, bf16[256,2048]{1,0:T(8,128)(2,1)S(1)} %get-tuple-element.36.k_ref.refs_2_, bf16[256,2048]{1,0:T(8,128)(2,1)S(1)} %get-tuple-element.38.v_ref.refs_4_, bf16[256,2048]{1,0:T(8,128)(2,1)S(1)} %get-tuple-element.34.refs_0_.q_ref), custom_call_target="tpu_custom_call" | custom-call | flops 134217728 | bytes 3145728 | tf_op jit(solution)/shard_map/core_states/pallas_call | solution.py:220
  8.3 0.0 collective-permute-done.1.k_sib_ref.refs_3_
  8.3 1.1 %collective-permute-done.2.v_sib_ref.refs_5_ = bf16[256,2048]{1,0:T(8,128)(2,1)S(1)} collective-permute-done((bf16[256,2048]{1,0:T(8,128)(2,1)S(1)}, bf16[256,2048]{1,0:T(8,128)(2,1)S(1)}, u32[]{:S(2)}, u32[]{:S(2)}) %collective-permute-start.2) | collective-permute-done | bytes 1048608 | tf_op jit(solution)/shard_map/ppermute | solution.py:539
  9.4 1.0 %chunk_states_0.1 = (f32[2,128,128]{2,1,0:T(8,128)S(1)}, f32[4,2,128,128]{3,2,1,0:T(8,128)S(1)}, s16[288,128]{1,0:T(8,128)(2,1)S(1)}, s16[272,128]{1,0:T(8,128)(2,1)S(1)}, s16[272,128]{1,0:T(8,128)(2,1)S(1)}) custom-call(s32[4]{0:T(128)S(1)} %pad_add_fusion.place_ref, f32[2,4,2,128,128]{4,3,2,1,0:T(8,128)S(1)} %core_states.1.mine_ref, ...), custom_call_target="tpu_custom_call" | custom-call | flops 67108864 | bytes 2359296 | tf_op jit(solution)/shard_map/chunk_states_0/pallas_call | solution.py:254
  10.4 3.9 %collective-permute-start.7 = (s16[272,128]{1,0:T(8,128)(2,1)S(1)}, s16[272,128]{1,0:T(8,128)(2,1)S(1)}, u32[]{:S(2)}, u32[]{:S(2)}) collective-permute-start(s16[272,128]{1,0:T(8,128)(2,1)S(1)} %get-tuple-element.47), channel_id=1, source_target_pairs={{0,6},{2,4},{4,2},{6,0},{1,7},{3,5},{5,3},{7,1},{8,14},{10,12},{12... | collective-permute-start | bytes 208904 | tf_op jit(solution)/shard_map/ppermute | solution.py:539
  14.3 0.5 collective-permute-start.3
  14.8 0.1 collective-permute-start.8
  15.0 0.0 collective-permute-done.refs_1_.refs_4_.q_sib_ref
  15.0 1.1 %chunk_states_1.1 = (f32[2,128,128]{2,1,0:T(8,128)S(1)}, f32[4,2,128,128]{3,2,1,0:T(8,128)S(1)}, s16[272,128]{1,0:T(8,128)(2,1)S(1)}, s16[272,128]{1,0:T(8,128)(2,1)S(1)}, s16[272,128]{1,0:T(8,128)(2,1)S(1)}) custom-call(s32[4]{0:T(128)S(1)} %pad_add_fusion.place_ref, f32[2,4,2,128,128]{4,3,2,1,0:T(8,128)S(1)} %core_states.1.mine_ref, ...), custom_call_target="tpu_custom_call" | custom-call | flops 67108864 | bytes 2359296 | tf_op jit(solution)/shard_map/chunk_states_1/pallas_call | solution.py:254
  16.0 2.0 %collective-permute-start.4 = (s16[272,128]{1,0:T(8,128)(2,1)S(1)}, s16[272,128]{1,0:T(8,128)(2,1)S(1)}, u32[]{:S(2)}, u32[]{:S(2)}) collective-permute-start(s16[272,128]{1,0:T(8,128)(2,1)S(1)} %get-tuple-element.44), channel_id=1, source_target_pairs={{0,2},{2,0},{4,6},{6,4},{1,3},{3,1},{5,7},{7,5},{8,10},{10,8},{12,... | collective-permute-start | bytes 208904 | tf_op jit(solution)/shard_map/ppermute | solution.py:539
  18.0 1.5 %collective-permute-start.5 = (s16[272,128]{1,0:T(8,128)(2,1)S(1)}, s16[272,128]{1,0:T(8,128)(2,1)S(1)}, u32[]{:S(2)}, u32[]{:S(2)}) collective-permute-start(s16[272,128]{1,0:T(8,128)(2,1)S(1)} %get-tuple-element.45), channel_id=1, source_target_pairs={{0,4},{2,6},{4,0},{6,2},{1,5},{3,7},{5,1},{7,3},{8,12},{10,14},{12... | collective-permute-start | bytes 208904 | tf_op jit(solution)/shard_map/ppermute | solution.py:539
  19.5 0.0 collective-permute-done.7.refs_0_.refs_2_.refs_3_
  19.5 0.7 collective-permute-start.6
  20.2 0.0 collective-permute-done.8.refs_1_.refs_2_
  20.2 0.0 collective-permute-done.3.refs_2_.refs_0_.refs_4_.refs_7_.refs_1_
  20.2 0.1 level_states_0.1
  20.3 3.5 %collective-permute-start.11 = (s16[272,128]{1,0:T(8,128)(2,1)S(1)}, s16[272,128]{1,0:T(8,128)(2,1)S(1)}, u32[]{:S(2)}, u32[]{:S(2)}) collective-permute-start(s16[272,128]{1,0:T(8,128)(2,1)S(1)} %get-tuple-element.49.refs_3_), channel_id=1, source_target_pairs={{0,8},{8,16},{16,24},{1,9},{9,17},{17,25},{2,10},{10,18},{18,26},{... | collective-permute-start | bytes 208904 | tf_op jit(solution)/shard_map/ppermute | solution.py:545
  23.8 0.0 collective-permute-done.4.refs_2_.refs_0_.refs_8_
  23.8 0.0 collective-permute-done.5.refs_1_.refs_9_
  23.8 0.9 %collective-permute-done.6.refs_0_.refs_2_.refs_10_ = s16[272,128]{1,0:T(8,128)(2,1)S(1)} collective-permute-done((s16[272,128]{1,0:T(8,128)(2,1)S(1)}, s16[272,128]{1,0:T(8,128)(2,1)S(1)}, u32[]{:S(2)}, u32[]{:S(2)}) %collective-permute-start.6) | collective-permute-done | bytes 69664 | tf_op jit(solution)/shard_map/ppermute | solution.py:539
  24.7 0.1 level_states_1.1
  24.8 3.5 %collective-permute-start.9 = (s16[272,128]{1,0:T(8,128)(2,1)S(1)}, s16[272,128]{1,0:T(8,128)(2,1)S(1)}, u32[]{:S(2)}, u32[]{:S(2)}) collective-permute-start(s16[272,128]{1,0:T(8,128)(2,1)S(1)} %get-tuple-element.50.refs_0_), channel_id=1, source_target_pairs={{0,8},{8,16},{16,24},{1,9},{9,17},{17,25},{2,10},{10,18},{18,26},{... | collective-permute-start | bytes 208904 | tf_op jit(solution)/shard_map/ppermute | solution.py:545
  28.3 4.5 %collective-permute-start.13 = (s16[272,128]{1,0:T(8,128)(2,1)S(1)}, s16[272,128]{1,0:T(8,128)(2,1)S(1)}, u32[]{:S(2)}, u32[]{:S(2)}) collective-permute-start(s16[272,128]{1,0:T(8,128)(2,1)S(1)} %get-tuple-element.49.refs_3_), channel_id=1, source_target_pairs={{0,16},{1,17},{2,18},{3,19},{4,20},{5,21},{6,22},{7,23}} | collective-permute-start | bytes 208904 | tf_op jit(solution)/shard_map/ppermute | solution.py:545
  32.8 0.0 collective-permute-done.11.before_ref.refs_3_.refs_4_
  32.8 0.1 two_levels_0.1.refs_0_
  32.9 0.7 collective-permute-start.14
  33.6 1.3 %collective-permute-start.10 = (s16[272,128]{1,0:T(8,128)(2,1)S(1)}, s16[272,128]{1,0:T(8,128)(2,1)S(1)}, u32[]{:S(2)}, u32[]{:S(2)}) collective-permute-start(s16[272,128]{1,0:T(8,128)(2,1)S(1)} %get-tuple-element.50.refs_0_), channel_id=1, source_target_pairs={{0,16},{1,17},{2,18},{3,19},{4,20},{5,21},{6,22},{7,23}} | collective-permute-start | bytes 208904 | tf_op jit(solution)/shard_map/ppermute | solution.py:545
  34.9 0.1 two_levels_1.1.refs_0_
  35.0 0.7 collective-permute-start.12
  35.6 1.5 %attend_local_0_1_3.1.refs_6_.refs_2_ = f32[2,256,512]{2,1,0:T(8,128)S(1)} custom-call(s32[4]{0:T(128)S(1)} %pad_add_fusion.place_ref, bf16[256,2048]{1,0:T(8,128)(2,1)S(1)} %get-tuple-element.34.refs_0_.q_ref, bf16[256,2048]{1,0:T(8,128)(2,1)S(1)} %collective-permute-done.refs_1_.refs_4_.q_sib_ref, bf16[256,2048]{1,0:T(8,128)(2,1)S(1)} %get-tuple-element.36.k_ref.refs_2_, ...), custom_call_target="tpu_custom_call" | custom-call | flops 268435456 | bytes 2097152 | tf_op jit(solution)/shard_map/attend_local_0_1_3/pallas_call | solution.py:392
  37.1 0.0 collective-permute-done.13.refs_4_.refs_5_
  37.1 0.8 %carries_0.1 = (s16[272,128]{1,0:T(8,128)(2,1)S(1)}, s16[272,128]{1,0:T(8,128)(2,1)S(1)}) custom-call(s32[4]{0:T(128)S(1)} %pad_add_fusion.place_ref, f32[2,128,128]{2,1,0:T(8,128)S(1)} %get-tuple-element.40.refs_0_.own_ref, s16[288,128]{1,0:T(8,128)(2,1)S(1)} %collective-permute-done.3.refs_2_.refs_0_.refs_4_.refs_7_.refs_1_, ...), custom_call_target="tpu_custom_call" | custom-call | bytes 1245184 | tf_op jit(solution)/shard_map/carries_0/pallas_call | solution.py:334
  37.9 0.8 %collective-permute-start.18 = (s16[272,128]{1,0:T(8,128)(2,1)S(1)}, s16[272,128]{1,0:T(8,128)(2,1)S(1)}, u32[]{:S(2)}, u32[]{:S(2)}) collective-permute-start(s16[272,128]{1,0:T(8,128)(2,1)S(1)} %get-tuple-element.57), channel_id=1, source_target_pairs={{0,6},{2,4},{4,2},{6,0},{1,7},{3,5},{5,3},{7,1},{8,14},{10,12},{12... | collective-permute-start | bytes 208904 | tf_op jit(solution)/shard_map/ppermute | solution.py:539
  38.7 1.3 %collective-permute-start.17 = (s16[272,128]{1,0:T(8,128)(2,1)S(1)}, s16[272,128]{1,0:T(8,128)(2,1)S(1)}, u32[]{:S(2)}, u32[]{:S(2)}) collective-permute-start(s16[272,128]{1,0:T(8,128)(2,1)S(1)} %get-tuple-element.53.refs_6_), channel_id=1, source_target_pairs={{0,2},{2,0},{4,6},{6,4},{1,3},{3,1},{5,7},{7,5},{8,10},{10,8},{12,... | collective-permute-start | bytes 208904 | tf_op jit(solution)/shard_map/ppermute | solution.py:539
  40.0 0.0 collective-permute-done.10.refs_4_.refs_12_
  40.0 0.0 collective-permute-done.12.refs_5_.refs_13_
  40.0 0.7 %carries_1.1 = (s16[272,128]{1,0:T(8,128)(2,1)S(1)}, s16[272,128]{1,0:T(8,128)(2,1)S(1)}) custom-call(s32[4]{0:T(128)S(1)} %pad_add_fusion.place_ref, f32[2,128,128]{2,1,0:T(8,128)S(1)} %get-tuple-element.43.refs_3_.own_ref.refs_7_, s16[272,128]{1,0:T(8,128)(2,1)S(1)} %collective-permute-done.4.refs_2_.refs_0_.refs_8_, ...), custom_call_target="tpu_custom_call" | custom-call | bytes 1245184 | tf_op jit(solution)/shard_map/carries_1/pallas_call | solution.py:334
  40.7 1.5 %collective-permute-start.16 = (s16[272,128]{1,0:T(8,128)(2,1)S(1)}, s16[272,128]{1,0:T(8,128)(2,1)S(1)}, u32[]{:S(2)}, u32[]{:S(2)}) collective-permute-start(s16[272,128]{1,0:T(8,128)(2,1)S(1)} %get-tuple-element.55), channel_id=1, source_target_pairs={{0,6},{2,4},{4,2},{6,0},{1,7},{3,5},{5,3},{7,1},{8,14},{10,12},{12... | collective-permute-start | bytes 208904 | tf_op jit(solution)/shard_map/ppermute | solution.py:539
  42.2 1.5 %collective-permute-start.15 = (s16[272,128]{1,0:T(8,128)(2,1)S(1)}, s16[272,128]{1,0:T(8,128)(2,1)S(1)}, u32[]{:S(2)}, u32[]{:S(2)}) collective-permute-start(s16[272,128]{1,0:T(8,128)(2,1)S(1)} %get-tuple-element.54.refs_7_), channel_id=1, source_target_pairs={{0,2},{2,0},{4,6},{6,4},{1,3},{3,1},{5,7},{7,5},{8,10},{10,8},{12,... | collective-permute-start | bytes 208904 | tf_op jit(solution)/shard_map/ppermute | solution.py:539
  43.7 0.0 collective-permute-done.17.refs_5_
  43.8 1.2 %attend_0_1_3.1.refs_10_ = bf16[512,512]{1,0:T(8,128)(2,1)S(1)} custom-call(s32[4]{0:T(128)S(1)} %pad_add_fusion.place_ref, bf16[256,2048]{1,0:T(8,128)(2,1)S(1)} %get-tuple-element.34.refs_0_.q_ref, bf16[256,2048]{1,0:T(8,128)(2,1)S(1)} %collective-permute-done.refs_1_.refs_4_.q_sib_ref, f32[2,256,512]{2,1,0:T(8,128)S(1)} %attend_local_0_1_3.1.refs_6_.refs_2_, ...), custom_call_target="tpu_custom_call" | custom-call | flops 402653184 | bytes 2097152 | tf_op jit(solution)/shard_map/attend_0_1_3/pallas_call | solution.py:464
  44.9 1.5 %collective-permute-start.21 = (bf16[512,512]{1,0:T(8,128)(2,1)S(1)}, bf16[512,512]{1,0:T(8,128)(2,1)S(1)}, u32[]{:S(2)}, u32[]{:S(2)}) collective-permute-start(bf16[512,512]{1,0:T(8,128)(2,1)S(1)} %attend_0_1_3.1.refs_10_), channel_id=1, source_target_pairs={{0,2},{2,0},{1,3},{3,1},{4,6},{6,4},{5,7},{7,5},{8,10},{10,8},{9,1... | collective-permute-start | bytes 1572872 | tf_op jit(solution)/shard_map/ppermute | solution.py:539
  46.4 0.0 collective-permute-done.16.refs_9_
  46.4 1.2 %collective-permute-done.15.refs_8_ = s16[272,128]{1,0:T(8,128)(2,1)S(1)} collective-permute-done((s16[272,128]{1,0:T(8,128)(2,1)S(1)}, s16[272,128]{1,0:T(8,128)(2,1)S(1)}, u32[]{:S(2)}, u32[]{:S(2)}) %collective-permute-start.15) | collective-permute-done | bytes 69664 | tf_op jit(solution)/shard_map/ppermute | solution.py:539
  47.7 1.9 %attend_1_1_3.1.refs_14_.refs_10_ = bf16[512,512]{1,0:T(8,128)(2,1)S(1)} custom-call(s32[4]{0:T(128)S(1)} %pad_add_fusion.place_ref, bf16[256,2048]{1,0:T(8,128)(2,1)S(1)} %get-tuple-element.34.refs_0_.q_ref, bf16[256,2048]{1,0:T(8,128)(2,1)S(1)} %collective-permute-done.refs_1_.refs_4_.q_sib_ref, bf16[256,2048]{1,0:T(8,128)(2,1)S(1)} %get-tuple-element.36.k_ref.refs_2_, ...), custom_call_target="tpu_custom_call" | custom-call | flops 402653184 | bytes 2097152 | tf_op jit(solution)/shard_map/attend_1_1_3/pallas_call | solution.py:464
  49.5 1.3 %collective-permute-start.19 = (bf16[512,512]{1,0:T(8,128)(2,1)S(1)}, bf16[512,512]{1,0:T(8,128)(2,1)S(1)}, u32[]{:S(2)}, u32[]{:S(2)}) collective-permute-start(bf16[512,512]{1,0:T(8,128)(2,1)S(1)} %attend_1_1_3.1.refs_14_.refs_10_), channel_id=1, source_target_pairs={{0,2},{2,0},{1,3},{3,1},{4,6},{6,4},{5,7},{7,5},{8,10},{10,8},{9,1... | collective-permute-start | bytes 1572872 | tf_op jit(solution)/shard_map/ppermute | solution.py:539
  50.8 1.1 %own_carries.1 = (s16[528,128]{1,0:T(8,128)(2,1)S(1)}, s16[528,128]{1,0:T(8,128)(2,1)S(1)}, f32[2,2,128,128]{3,2,1,0:T(8,128)S(1)}, f32[2,2,128,128]{3,2,1,0:T(8,128)S(1)}) custom-call(s32[4]{0:T(128)S(1)} %pad_add_fusion.place_ref, f32[2,128,128]{2,1,0:T(8,128)S(1)} %get-tuple-element.40.refs_0_.own_ref, ...), custom_call_target="tpu_custom_call" | custom-call | bytes 2621440 | tf_op jit(solution)/shard_map/own_carries/pallas_call | solution.py:368
  51.9 0.8 %collective-permute-start.22 = (f32[2,2,128,128]{3,2,1,0:T(8,128)S(1)}, f32[2,2,128,128]{3,2,1,0:T(8,128)S(1)}, u32[]{:S(2)}, u32[]{:S(2)}) collective-permute-start(f32[2,2,128,128]{3,2,1,0:T(8,128)S(1)} %get-tuple-element.61), channel_id=1, source_target_pairs={{0,4},{4,0},{1,5},{5,1},{2,6},{6,2},{3,7},{7,3},{8,12},{12,8},{9,1... | collective-permute-start | bytes 786440 | tf_op jit(solution)/shard_map/ppermute | solution.py:539
  52.7 1.2 %collective-permute-start.20 = (s16[528,128]{1,0:T(8,128)(2,1)S(1)}, s16[528,128]{1,0:T(8,128)(2,1)S(1)}, u32[]{:S(2)}, u32[]{:S(2)}) collective-permute-start(s16[528,128]{1,0:T(8,128)(2,1)S(1)} %get-tuple-element.59), channel_id=1, source_target_pairs={{0,4},{2,6},{4,0},{6,2},{1,5},{3,7},{5,1},{7,3},{8,12},{10,14},{12... | collective-permute-start | bytes 405512 | tf_op jit(solution)/shard_map/ppermute | solution.py:539
  54.0 5.8 %collective-permute-done.20.refs_9_ = s16[528,128]{1,0:T(8,128)(2,1)S(1)} collective-permute-done((s16[528,128]{1,0:T(8,128)(2,1)S(1)}, s16[528,128]{1,0:T(8,128)(2,1)S(1)}, u32[]{:S(2)}, u32[]{:S(2)}) %collective-permute-start.20) | collective-permute-done | bytes 135200 | tf_op jit(solution)/shard_map/ppermute | solution.py:539
  59.8 1.9 %attend_0_0_2.1.refs_10_.refs_0_ = bf16[512,512]{1,0:T(8,128)(2,1)S(1)} custom-call(s32[4]{0:T(128)S(1)} %pad_add_fusion.place_ref, bf16[256,2048]{1,0:T(8,128)(2,1)S(1)} %get-tuple-element.34.refs_0_.q_ref, bf16[256,2048]{1,0:T(8,128)(2,1)S(1)} %collective-permute-done.refs_1_.refs_4_.q_sib_ref, bf16[256,2048]{1,0:T(8,128)(2,1)S(1)} %get-tuple-element.36.k_ref.refs_2_, ...), custom_call_target="tpu_custom_call" | custom-call | flops 402653184 | bytes 2097152 | tf_op jit(solution)/shard_map/attend_0_0_2/pallas_call | solution.py:464
  61.7 1.9 %attend_1_0_2.1.refs_1_ = bf16[512,512]{1,0:T(8,128)(2,1)S(1)} custom-call(s32[4]{0:T(128)S(1)} %pad_add_fusion.place_ref, bf16[256,2048]{1,0:T(8,128)(2,1)S(1)} %get-tuple-element.34.refs_0_.q_ref, bf16[256,2048]{1,0:T(8,128)(2,1)S(1)} %collective-permute-done.refs_1_.refs_4_.q_sib_ref, bf16[256,2048]{1,0:T(8,128)(2,1)S(1)} %get-tuple-element.36.k_ref.refs_2_, ...), custom_call_target="tpu_custom_call" | custom-call | flops 402653184 | bytes 2097152 | tf_op jit(solution)/shard_map/attend_1_0_2/pallas_call | solution.py:464
  63.5 0.0 collective-permute-done.22.refs_1_
  63.5 1.4 %assemble_cache.1 = f32[1,8,128,128]{3,2,1,0:T(8,128)} custom-call(s32[4]{0:T(128)S(1)} %pad_add_fusion.place_ref, f32[2,2,128,128]{3,2,1,0:T(8,128)S(1)} %get-tuple-element.60.refs_0_, f32[2,2,128,128]{3,2,1,0:T(8,128)S(1)} %collective-permute-done.22.refs_1_), custom_call_target="tpu_custom_call" | custom-call | tf_op jit(solution)/shard_map/assemble_cache/pallas_call | solution.py:524
  64.9 0.0 collective-permute-done.21.refs_2_
  64.9 1.7 %assemble.1.refs_1_ = bf16[1024,1024]{1,0:T(8,128)(2,1)} custom-call(s32[4]{0:T(128)S(1)} %pad_add_fusion.place_ref, bf16[512,512]{1,0:T(8,128)(2,1)S(1)} %attend_0_0_2.1.refs_10_.refs_0_, bf16[512,512]{1,0:T(8,128)(2,1)S(1)} %attend_1_0_2.1.refs_1_, bf16[512,512]{1,0:T(8,128)(2,1)S(1)} %collective-permute-done.21.refs_2_), custom_call_target="tpu_custom_call" | custom-call | tf_op jit(solution)/shard_map/assemble/pallas_call | solution.py:503
  66.7 1.3 %collective-permute-done.19.refs_0_ = bf16[512,512]{1,0:T(8,128)(2,1)S(1)} collective-permute-done((bf16[512,512]{1,0:T(8,128)(2,1)S(1)}, bf16[512,512]{1,0:T(8,128)(2,1)S(1)}, u32[]{:S(2)}, u32[]{:S(2)}) %collective-permute-start.19) | collective-permute-done | bytes 524320 | tf_op jit(solution)/shard_map/ppermute | solution.py:539
  68.0 1.4 %finish.1 = bf16[1024,1024]{1,0:T(8,128)(2,1)} custom-call(s32[4]{0:T(128)S(1)} %pad_add_fusion.place_ref, bf16[512,512]{1,0:T(8,128)(2,1)S(1)} %collective-permute-done.19.refs_0_, bf16[1024,1024]{1,0:T(8,128)(2,1)} %assemble.1.refs_1_), custom_call_target="tpu_custom_call", output_to_operand_aliasing={{}: (2, {})} | custom-call | tf_op jit(solution)/shard_map/finish/pallas_call | solution.py:503
  (7 shorter events, 0.0 us)
Async XLA Ops:
  0.7 5.0 %copy-start = (bf16[256,4096]{1,0:T(8,128)(2,1)S(1)}, bf16[256,4096]{1,0:T(8,128)(2,1)}, u32[]{:S(2)}) copy-start(bf16[256,4096]{1,0:T(8,128)(2,1)} %queries_ref.1) | copy-start | bytes 6291460
  5.1 3.2 %collective-permute-start.1 = (bf16[256,2048]{1,0:T(8,128)(2,1)S(1)}, bf16[256,2048]{1,0:T(8,128)(2,1)S(1)}, u32[]{:S(2)}, u32[]{:S(2)}) collective-permute-start(bf16[256,2048]{1,0:T(8,128)(2,1)S(1)} %get-tuple-element.37), channel_id=1, source_target_pairs={{0,1},{1,0},{2,3},{3,2},{4,5},{5,4},{6,7},{7,6},{8,9},{9,8},{10,11... | collective-permute-start | bytes 3145736 | tf_op jit(solution)/shard_map/ppermute | solution.py:539
  5.6 3.8 %collective-permute-start.2 = (bf16[256,2048]{1,0:T(8,128)(2,1)S(1)}, bf16[256,2048]{1,0:T(8,128)(2,1)S(1)}, u32[]{:S(2)}, u32[]{:S(2)}) collective-permute-start(bf16[256,2048]{1,0:T(8,128)(2,1)S(1)} %get-tuple-element.39), channel_id=1, source_target_pairs={{0,1},{1,0},{2,3},{3,2},{4,5},{5,4},{6,7},{7,6},{8,9},{9,8},{10,11... | collective-permute-start | bytes 3145736 | tf_op jit(solution)/shard_map/ppermute | solution.py:539
  6.4 8.5 %collective-permute-start = (bf16[256,2048]{1,0:T(8,128)(2,1)S(1)}, bf16[256,2048]{1,0:T(8,128)(2,1)S(1)}, u32[]{:S(2)}, u32[]{:S(2)}) collective-permute-start(bf16[256,2048]{1,0:T(8,128)(2,1)S(1)} %get-tuple-element.35), channel_id=1, source_target_pairs={{0,1},{1,0},{2,3},{3,2},{4,5},{5,4},{6,7},{7,6},{8,9},{9,8},{10,11... | collective-permute-start | bytes 3145736 | tf_op jit(solution)/shard_map/ppermute | solution.py:539
  6.9 2.5 %copy-start.1 = (f32[1024]{0:T(1024)S(1)}, f32[1024]{0:T(1024)}, u32[]{:S(2)}) copy-start(f32[1024]{0:T(1024)} %param.9) | copy-start | bytes 12292
  10.4 9.1 %collective-permute-start.7 = (s16[272,128]{1,0:T(8,128)(2,1)S(1)}, s16[272,128]{1,0:T(8,128)(2,1)S(1)}, u32[]{:S(2)}, u32[]{:S(2)}) collective-permute-start(s16[272,128]{1,0:T(8,128)(2,1)S(1)} %get-tuple-element.47), channel_id=1, source_target_pairs={{0,6},{2,4},{4,2},{6,0},{1,7},{3,5},{5,3},{7,1},{8,14},{10,12},{12... | collective-permute-start | bytes 208904 | tf_op jit(solution)/shard_map/ppermute | solution.py:539
  14.3 5.9 %collective-permute-start.3 = (s16[288,128]{1,0:T(8,128)(2,1)S(1)}, s16[288,128]{1,0:T(8,128)(2,1)S(1)}, u32[]{:S(2)}, u32[]{:S(2)}) collective-permute-start(s16[288,128]{1,0:T(8,128)(2,1)S(1)} %get-tuple-element.42), channel_id=1, source_target_pairs={{0,2},{2,0},{4,6},{6,4},{1,3},{3,1},{5,7},{7,5},{8,10},{10,8},{12,... | collective-permute-start | bytes 221192 | tf_op jit(solution)/shard_map/ppermute | solution.py:539
  14.8 5.4 %collective-permute-start.8 = (s16[272,128]{1,0:T(8,128)(2,1)S(1)}, s16[272,128]{1,0:T(8,128)(2,1)S(1)}, u32[]{:S(2)}, u32[]{:S(2)}) collective-permute-start(s16[272,128]{1,0:T(8,128)(2,1)S(1)} %get-tuple-element.48), channel_id=1, source_target_pairs={{0,4},{2,6},{4,0},{6,2},{1,5},{3,7},{5,1},{7,3},{8,12},{10,14},{12... | collective-permute-start | bytes 208904 | tf_op jit(solution)/shard_map/ppermute | solution.py:539
  16.0 7.8 %collective-permute-start.4 = (s16[272,128]{1,0:T(8,128)(2,1)S(1)}, s16[272,128]{1,0:T(8,128)(2,1)S(1)}, u32[]{:S(2)}, u32[]{:S(2)}) collective-permute-start(s16[272,128]{1,0:T(8,128)(2,1)S(1)} %get-tuple-element.44), channel_id=1, source_target_pairs={{0,2},{2,0},{4,6},{6,4},{1,3},{3,1},{5,7},{7,5},{8,10},{10,8},{12,... | collective-permute-start | bytes 208904 | tf_op jit(solution)/shard_map/ppermute | solution.py:539
  18.0 5.8 %collective-permute-start.5 = (s16[272,128]{1,0:T(8,128)(2,1)S(1)}, s16[272,128]{1,0:T(8,128)(2,1)S(1)}, u32[]{:S(2)}, u32[]{:S(2)}) collective-permute-start(s16[272,128]{1,0:T(8,128)(2,1)S(1)} %get-tuple-element.45), channel_id=1, source_target_pairs={{0,4},{2,6},{4,0},{6,2},{1,5},{3,7},{5,1},{7,3},{8,12},{10,14},{12... | collective-permute-start | bytes 208904 | tf_op jit(solution)/shard_map/ppermute | solution.py:539
  19.5 5.2 %collective-permute-start.6 = (s16[272,128]{1,0:T(8,128)(2,1)S(1)}, s16[272,128]{1,0:T(8,128)(2,1)S(1)}, u32[]{:S(2)}, u32[]{:S(2)}) collective-permute-start(s16[272,128]{1,0:T(8,128)(2,1)S(1)} %get-tuple-element.46), channel_id=1, source_target_pairs={{0,6},{2,4},{4,2},{6,0},{1,7},{3,5},{5,3},{7,1},{8,14},{10,12},{12... | collective-permute-start | bytes 208904 | tf_op jit(solution)/shard_map/ppermute | solution.py:539
  20.3 12.5 %collective-permute-start.11 = (s16[272,128]{1,0:T(8,128)(2,1)S(1)}, s16[272,128]{1,0:T(8,128)(2,1)S(1)}, u32[]{:S(2)}, u32[]{:S(2)}) collective-permute-start(s16[272,128]{1,0:T(8,128)(2,1)S(1)} %get-tuple-element.49.refs_3_), channel_id=1, source_target_pairs={{0,8},{8,16},{16,24},{1,9},{9,17},{17,25},{2,10},{10,18},{18,26},{... | collective-permute-start | bytes 208904 | tf_op jit(solution)/shard_map/ppermute | solution.py:545
  24.8 10.1 %collective-permute-start.9 = (s16[272,128]{1,0:T(8,128)(2,1)S(1)}, s16[272,128]{1,0:T(8,128)(2,1)S(1)}, u32[]{:S(2)}, u32[]{:S(2)}) collective-permute-start(s16[272,128]{1,0:T(8,128)(2,1)S(1)} %get-tuple-element.50.refs_0_), channel_id=1, source_target_pairs={{0,8},{8,16},{16,24},{1,9},{9,17},{17,25},{2,10},{10,18},{18,26},{... | collective-permute-start | bytes 208904 | tf_op jit(solution)/shard_map/ppermute | solution.py:545
  28.3 8.8 %collective-permute-start.13 = (s16[272,128]{1,0:T(8,128)(2,1)S(1)}, s16[272,128]{1,0:T(8,128)(2,1)S(1)}, u32[]{:S(2)}, u32[]{:S(2)}) collective-permute-start(s16[272,128]{1,0:T(8,128)(2,1)S(1)} %get-tuple-element.49.refs_3_), channel_id=1, source_target_pairs={{0,16},{1,17},{2,18},{3,19},{4,20},{5,21},{6,22},{7,23}} | collective-permute-start | bytes 208904 | tf_op jit(solution)/shard_map/ppermute | solution.py:545
  32.9 4.2 %collective-permute-start.14 = (s16[272,128]{1,0:T(8,128)(2,1)S(1)}, s16[272,128]{1,0:T(8,128)(2,1)S(1)}, u32[]{:S(2)}, u32[]{:S(2)}) collective-permute-start(s16[272,128]{1,0:T(8,128)(2,1)S(1)} %two_levels_0.1.refs_0_), channel_id=1, source_target_pairs={{8,24},{9,25},{10,26},{11,27},{12,28},{13,29},{14,30},{15,31}} | collective-permute-start | bytes 208904 | tf_op jit(solution)/shard_map/ppermute | solution.py:545
  33.6 6.4 %collective-permute-start.10 = (s16[272,128]{1,0:T(8,128)(2,1)S(1)}, s16[272,128]{1,0:T(8,128)(2,1)S(1)}, u32[]{:S(2)}, u32[]{:S(2)}) collective-permute-start(s16[272,128]{1,0:T(8,128)(2,1)S(1)} %get-tuple-element.50.refs_0_), channel_id=1, source_target_pairs={{0,16},{1,17},{2,18},{3,19},{4,20},{5,21},{6,22},{7,23}} | collective-permute-start | bytes 208904 | tf_op jit(solution)/shard_map/ppermute | solution.py:545
  35.0 5.0 %collective-permute-start.12 = (s16[272,128]{1,0:T(8,128)(2,1)S(1)}, s16[272,128]{1,0:T(8,128)(2,1)S(1)}, u32[]{:S(2)}, u32[]{:S(2)}) collective-permute-start(s16[272,128]{1,0:T(8,128)(2,1)S(1)} %two_levels_1.1.refs_0_), channel_id=1, source_target_pairs={{8,24},{9,25},{10,26},{11,27},{12,28},{13,29},{14,30},{15,31}} | collective-permute-start | bytes 208904 | tf_op jit(solution)/shard_map/ppermute | solution.py:545
  37.9 5.8 %collective-permute-start.18 = (s16[272,128]{1,0:T(8,128)(2,1)S(1)}, s16[272,128]{1,0:T(8,128)(2,1)S(1)}, u32[]{:S(2)}, u32[]{:S(2)}) collective-permute-start(s16[272,128]{1,0:T(8,128)(2,1)S(1)} %get-tuple-element.57), channel_id=1, source_target_pairs={{0,6},{2,4},{4,2},{6,0},{1,7},{3,5},{5,3},{7,1},{8,14},{10,12},{12... | collective-permute-start | bytes 208904 | tf_op jit(solution)/shard_map/ppermute | solution.py:539
  38.7 5.1 %collective-permute-start.17 = (s16[272,128]{1,0:T(8,128)(2,1)S(1)}, s16[272,128]{1,0:T(8,128)(2,1)S(1)}, u32[]{:S(2)}, u32[]{:S(2)}) collective-permute-start(s16[272,128]{1,0:T(8,128)(2,1)S(1)} %get-tuple-element.53.refs_6_), channel_id=1, source_target_pairs={{0,2},{2,0},{4,6},{6,4},{1,3},{3,1},{5,7},{7,5},{8,10},{10,8},{12,... | collective-permute-start | bytes 208904 | tf_op jit(solution)/shard_map/ppermute | solution.py:539
  40.7 5.7 %collective-permute-start.16 = (s16[272,128]{1,0:T(8,128)(2,1)S(1)}, s16[272,128]{1,0:T(8,128)(2,1)S(1)}, u32[]{:S(2)}, u32[]{:S(2)}) collective-permute-start(s16[272,128]{1,0:T(8,128)(2,1)S(1)} %get-tuple-element.55), channel_id=1, source_target_pairs={{0,6},{2,4},{4,2},{6,0},{1,7},{3,5},{5,3},{7,1},{8,14},{10,12},{12... | collective-permute-start | bytes 208904 | tf_op jit(solution)/shard_map/ppermute | solution.py:539
  42.2 5.4 %collective-permute-start.15 = (s16[272,128]{1,0:T(8,128)(2,1)S(1)}, s16[272,128]{1,0:T(8,128)(2,1)S(1)}, u32[]{:S(2)}, u32[]{:S(2)}) collective-permute-start(s16[272,128]{1,0:T(8,128)(2,1)S(1)} %get-tuple-element.54.refs_7_), channel_id=1, source_target_pairs={{0,2},{2,0},{4,6},{6,4},{1,3},{3,1},{5,7},{7,5},{8,10},{10,8},{12,... | collective-permute-start | bytes 208904 | tf_op jit(solution)/shard_map/ppermute | solution.py:539
  44.9 20.0 %collective-permute-start.21 = (bf16[512,512]{1,0:T(8,128)(2,1)S(1)}, bf16[512,512]{1,0:T(8,128)(2,1)S(1)}, u32[]{:S(2)}, u32[]{:S(2)}) collective-permute-start(bf16[512,512]{1,0:T(8,128)(2,1)S(1)} %attend_0_1_3.1.refs_10_), channel_id=1, source_target_pairs={{0,2},{2,0},{1,3},{3,1},{4,6},{6,4},{5,7},{7,5},{8,10},{10,8},{9,1... | collective-permute-start | bytes 1572872 | tf_op jit(solution)/shard_map/ppermute | solution.py:539
  49.5 18.5 %collective-permute-start.19 = (bf16[512,512]{1,0:T(8,128)(2,1)S(1)}, bf16[512,512]{1,0:T(8,128)(2,1)S(1)}, u32[]{:S(2)}, u32[]{:S(2)}) collective-permute-start(bf16[512,512]{1,0:T(8,128)(2,1)S(1)} %attend_1_1_3.1.refs_14_.refs_10_), channel_id=1, source_target_pairs={{0,2},{2,0},{1,3},{3,1},{4,6},{6,4},{5,7},{7,5},{8,10},{10,8},{9,1... | collective-permute-start | bytes 1572872 | tf_op jit(solution)/shard_map/ppermute | solution.py:539
  51.9 11.6 %collective-permute-start.22 = (f32[2,2,128,128]{3,2,1,0:T(8,128)S(1)}, f32[2,2,128,128]{3,2,1,0:T(8,128)S(1)}, u32[]{:S(2)}, u32[]{:S(2)}) collective-permute-start(f32[2,2,128,128]{3,2,1,0:T(8,128)S(1)} %get-tuple-element.61), channel_id=1, source_target_pairs={{0,4},{4,0},{1,5},{5,1},{2,6},{6,2},{3,7},{7,3},{8,12},{12,8},{9,1... | collective-permute-start | bytes 786440 | tf_op jit(solution)/shard_map/ppermute | solution.py:539
  52.7 7.0 %collective-permute-start.20 = (s16[528,128]{1,0:T(8,128)(2,1)S(1)}, s16[528,128]{1,0:T(8,128)(2,1)S(1)}, u32[]{:S(2)}, u32[]{:S(2)}) collective-permute-start(s16[528,128]{1,0:T(8,128)(2,1)S(1)} %get-tuple-element.59), channel_id=1, source_target_pairs={{0,4},{2,6},{4,0},{6,2},{1,5},{3,7},{5,1},{7,3},{8,12},{10,14},{12... | collective-permute-start | bytes 405512 | tf_op jit(solution)/shard_map/ppermute | solution.py:539

commit v13 on v11

--- a/solution.py
+++ b/solution.py
@@ -44,6 +44,7 @@
         self.rows = rows
         self.block = rows * n_head
         self.piece = self.each * HD
+        self.half_width = self.width // self.halves
 
 
 def counts_of(spikes):
@@ -60,20 +61,25 @@
 
 
 def sides(plan, place_ref):
+    width = plan.half_width
     for y in range(plan.n_y):
         for side in range(CORES):
             of = place_ref[0] if side == 0 else 1 - place_ref[0]
-            start = pl.multiple_of((y * CORES + of) * plan.width, plan.width)
-            yield side, slice(y * plan.width, (y + 1) * plan.width), pl.ds(start, plan.width)
+            for half in range(plan.halves):
+                start = ((y * CORES + of) * plan.halves + half) * width
+                at = pl.ds(pl.multiple_of(start, width), width)
+                yield side, half, slice(y * width, (y + 1) * width), at
 
 
 def decode(plan, place, spikes, keys, values):
     rows, model = spikes.shape
     step = min(rows, 32)
     chunks = rows // step
+    n_out = 3 * CORES * plan.halves
 
     def kernel(place_ref, *refs):
-        sources, outs, buffers, sems = refs[:3], refs[3:9], refs[9:12], refs[12]
+        sources, *outs, b0, b1, b2, sems = refs[:3], *refs[3:]
+        buffers = (b0, b1, b2)
 
         def fetch(chunk, index):
             at = pl.ds(chunk * step, step)
@@ -90,18 +96,18 @@
             for index in range(3):
                 fetch(chunk, index).wait()
             at = pl.ds(pl.multiple_of(chunk * step, step), step)
-            for side, mine, columns in sides(plan, place_ref):
+            for side, half, mine, columns in sides(plan, place_ref):
                 spikes = buffers[0][at, columns].astype(jnp.float32).astype(jnp.bfloat16)
                 value, key, query = counts_of(spikes)
-                outs[side][at, mine] = buffers[1][at, columns] * key
-                outs[2 + side][at, mine] = buffers[2][at, columns] * value
-                outs[4 + side][at, mine] = query
-
-    return pl.pallas_call(
-        kernel,
-        out_shape=[jax.ShapeDtypeStruct((rows, plan.n_y * plan.width), jnp.bfloat16)] * 6,
+                spiked = (buffers[1][at, columns] * key, buffers[2][at, columns] * value, query)
+                for index, array in enumerate(spiked):
+                    outs[(index * CORES + side) * plan.halves + half][at, mine] = array
+
+    return pl.pallas_call(
+        kernel,
+        out_shape=[jax.ShapeDtypeStruct((rows, plan.n_y * plan.half_width), jnp.bfloat16)] * n_out,
         in_specs=[SMEM] + [HBM] * 3,
-        out_specs=[VMEM] * 6,
+        out_specs=[VMEM] * n_out,
         scratch_shapes=[
             pltpu.VMEM((rows, model), jnp.int32),
             pltpu.VMEM((rows, model), jnp.bfloat16),
@@ -115,15 +121,18 @@
 
 
 def spike_queries(plan, place, queries, counts):
+    n = len(counts)
+
     def kernel(place_ref, queries_ref, *refs):
-        for side, mine, columns in sides(plan, place_ref):
-            refs[2 + side][:, mine] = queries_ref[:, columns] * refs[side][:, mine]
+        for side, half, mine, columns in sides(plan, place_ref):
+            at = side * plan.halves + half
+            refs[n + at][:, mine] = queries_ref[:, columns] * refs[at][:, mine]
 
     return pl.pallas_call(
         kernel,
         out_shape=[jax.ShapeDtypeStruct(a.shape, jnp.bfloat16) for a in counts],
-        in_specs=[SMEM] + [VMEM] * 3,
-        out_specs=[VMEM] * 2,
+        in_specs=[SMEM] + [VMEM] * (1 + n),
+        out_specs=[VMEM] * n,
         compiler_params=params(),
         cost_estimate=cost(queries.size, queries.size * 6),
         name="spike_queries",
@@ -201,30 +210,29 @@
     return jax.ShapeDtypeStruct((*lead, HD, HD), jnp.float32)
 
 
-def owned_columns(plan, place_ref, offset, half, i):
+def owned_columns(plan, place_ref, offset, i):
     x = place_ref[1] ^ (offset // plan.n_y)
     y = place_ref[2] ^ (offset % plan.n_y)
-    start = (((y * plan.halves + half) * plan.n_inner + x) * plan.each + i) * HD
+    start = ((y * plan.n_inner + x) * plan.each + i) * HD
     return pl.ds(pl.multiple_of(start, HD), HD)
 
 
-def core_states(plan, place, key, value, after):
+def core_states(plan, place, key, value, half, after):
     def kernel(place_ref, k_ref, v_ref, *refs):
-        for half in range(plan.halves):
-            for offset in range(plan.plane):
-                for i in range(plan.each):
-                    at = owned_columns(plan, place_ref, offset, half, i)
-                    refs[-1][half, offset, i] = contract_rows(v_ref[:, at], k_ref[:, at])
-
-    heads = plan.halves * plan.plane * plan.each
-    return pl.pallas_call(
-        kernel,
-        out_shape=states_shape(plan.halves, plan.plane, plan.each),
+        for offset in range(plan.plane):
+            for i in range(plan.each):
+                at = owned_columns(plan, place_ref, offset, i)
+                refs[-1][offset, i] = contract_rows(v_ref[:, at], k_ref[:, at])
+
+    heads = plan.plane * plan.each
+    return pl.pallas_call(
+        kernel,
+        out_shape=states_shape(plan.plane, plan.each),
         in_specs=[SMEM] + [VMEM] * 2 + [ANY] * len(after),
         out_specs=VMEM,
         compiler_params=params(),
         cost_estimate=cost(2 * plan.rows * HD * HD * heads, 4 * heads * HD * (plan.rows + HD)),
-        name="core_states",
+        name=f"core_states_{half}",
     )(place, key, value, *after)
 
 
@@ -237,8 +245,8 @@
         for offset in (*range(1, plan.plane), 0):
             states = []
             for i in range(plan.each):
-                at = owned_columns(plan, place_ref, offset, half, i)
-                mine = mine_ref[half, offset, i]
+                at = owned_columns(plan, place_ref, offset, i)
+                mine = mine_ref[offset, i]
                 sib = contract_rows(v_sib_ref[:, at], k_sib_ref[:, at])
                 first_ref[offset, i] = jnp.where(is_first, mine, sib)
                 states.append(mine + sib)
@@ -365,7 +373,7 @@
     def kernel(place_ref, q_ref, q_sib_ref, k_ref, k_sib_ref, v_ref, v_sib_ref, *refs):
         for piece, offset in enumerate(offsets):
             for i in range(plan.each):
-                at = owned_columns(plan, place_ref, offset, half, i)
+                at = owned_columns(plan, place_ref, offset, i)
                 out_at = slice(piece * plan.piece + i * HD, piece * plan.piece + (i + 1) * HD)
                 refs[-1][0, :, out_at] = local_part(q_ref, k_ref, v_ref, at)
                 refs[-1][1, :, out_at] = local_part(q_sib_ref, k_sib_ref, v_sib_ref, at)
@@ -421,7 +429,7 @@
             carry_states = decoded(carry_refs[piece])
             skip = half * plan.each if len(carry_states) > plan.each else 0
             for i in range(plan.each):
-                at = owned_columns(plan, place_ref, offset, half, i)
+                at = owned_columns(plan, place_ref, offset, i)
                 head = (half * plan.n_inner + x) * plan.each + i
                 if coded_gain:
                     gain = jnp.where(line == head, decoded_gain(gain_ref), 0.0)
@@ -528,19 +536,30 @@
         return lax.ppermute(array, "outer", pairs)
 
     gain = gain.reshape(1, plan.width)
-    key, key_out, value, value_out, *counts = decode(plan, place, spikes, keys, values)
-    key, value = ((a, swap(b, "core", 1, CORES)) for a, b in ((key, key_out), (value, value_out)))
-    query, query_out = spike_queries(plan, place, queries, counts)
-    query = (query, swap(query_out, "core", 1, CORES))
-
-    of_core = core_states(plan, place, key[0], value[0], [query[0]])
+    arrays = decode(plan, place, spikes, keys, values)
+    parts = [arrays[k : k + plan.halves] for k in range(0, len(arrays), plan.halves)]
+
+    def with_siblings(mine, theirs):
+        return [(a, swap(b, "core", 1, CORES)) for a, b in zip(mine, theirs)]
+
+    key, value = with_siblings(*parts[0:2]), with_siblings(*parts[2:4])
+    spiked = spike_queries(plan, place, queries, [*parts[4], *parts[5]])
+    query = with_siblings(spiked[: plan.halves], spiked[plan.halves :])
+
+    after = [query[0][0]]
+    of_core = []
+    for half in halves:
+        of_core.append(core_states(plan, place, key[half][0], value[half][0], half, after))
+        after = [of_core[half]]
     own, first, others = [], [], []
 
     def owner_stage(half, after):
         with_gain = gain if half == 0 else None
-        mine, parts, *sends = chunk_states(plan, place, of_core, key[1], value[1], half, after, with_gain)
+        mine, of_first, *sends = chunk_states(
+            plan, place, of_core[half], key[half][1], value[half][1], half, after, with_gain
+        )
         own.append(mine)
-        first.append(parts)
+        first.append(of_first)
         others.append([in_level(a, o) for o, a in enumerate(sends, 1)])
 
     of_group = [list(range(y, plan.plane, plan.n_y)) for y in range(plan.n_y)]
@@ -550,9 +569,9 @@
         return attend(
             plan,
             place,
-            query,
-            key,
-            value,
+            query[half],
+            key[half],
+            value[half],
             [carry[o] for o in offsets],
             first[half],
             others[0][offsets[0] % plan.n_y - 1] if offsets[0] % plan.n_y else gain,
@@ -578,21 +597,21 @@
     after = []
     for half in halves:
         owner_stage(half, after)
-        after = [own[-1], query[1]]
+        after = [own[-1], *[a for _, a in query]]
     levels = []
     for half in halves:
         level = level_states(plan, own[half], others[half][::-1], half, after)
         levels.append([to_later(level, d) for d in range(1, plan.n_outer)])
         after = [level]
-    local = {}
-    for y in range(1, plan.n_y):
-        local[y] = attend_local(plan, place, query, key, value, 0, of_group[y], after)
-        after = [local[y]]
-    carry = []
+    carry, local = [], {}
     for half in halves:
         done, of_half = carry_stage(half, after)
         carry.append(of_half)
         after = [done]
+        for y in range(1, plan.n_y):
+            if half == 0:
+                local[y] = attend_local(plan, place, query[0], key[0], value[0], 0, of_group[y], after)
+                after = [local[y]]
     for half in halves:
         after = send_stage(half, carry[half], after, {} if half else local)
     sends = own_carries(plan, place, own, others, levels, of_group[0], after)

time: 68.9 us -> 68.5 us (level)
  waiting for transfers between devices: 10.2 us -> 8.8 us
  Pallas kernels: 24.1 us -> 24.8 us
    ppermute x17 -> x20, waiting for transfers between devices: 10.2 us -> 8.79 us  [swap(): return lax.ppermute(array, axes, [(i, i ^ offset) for i in range(size)])]
    ppermute x6, starting transfers between devices: 13.4 us -> 14.2 us  [to_later(): return lax.ppermute(array, 'outer', pairs)]
    ppermute x17 -> x20, starting transfers between devices: 20.1 us -> 19.3 us  [swap(): return lax.ppermute(array, axes, [(i, i ^ offset) for i in range(size)])]
    pallas_call x1 -> x2, Pallas kernels: 1.36 us -> 2.03 us  [core_states(): pl.pallas_call(kernel, out_shape=states_shape(plan.plane, plan.each), in_...]
  transfers between devices with their start and end apart: 23 -> 26, of which waited for: 5 -> 5; matrix products, arithmetic and copies ran while one was open for 0% -> 0% of each run, Pallas kernels for 27% -> 28%
where the time goes in v13:
time: 68.5 us; the launch traced here: 68.2 us
  starting transfers between devices  33.6 us (49%)
  Pallas kernels  24.8 us (36%)
  waiting for transfers between devices  8.8 us (13%)
  between operations  0.92 us (1%)
    ppermute x20, starting transfers between devices, swap(): return lax.ppermute(array, axes, [(i, i ^ offset) for i in range(size)])  19.3 us
    ppermute x6, starting transfers between devices, to_later(): return lax.ppermute(array, 'outer', pairs)  14.2 us
    ppermute x20, waiting for transfers between devices, swap(): return lax.ppermute(array, axes, [(i, i ^ offset) for i in range(size)])  8.79 us
    pallas_call x4, Pallas kernels, attend(): pl.pallas_call(kernel, out_shape=jax.ShapeDtypeStruct((CORES * rows, head...  6.79 us
    pallas_call x1, Pallas kernels, decode(): pl.pallas_call(kernel, out_shape=[jax.ShapeDtypeStruct((rows, plan.n_y *...  4.36 us
    pallas_call x2, Pallas kernels, assemble(): pl.pallas_call(kernel, out_shape=jax.ShapeDtypeStruct((plan.n_y * rows, p...  3.08 us
    pallas_call x2, Pallas kernels, chunk_states(): pl.pallas_call(kernel, out_shape=[states_shape(plan.each), states_shape(p...  2.09 us
    pallas_call x2, Pallas kernels, core_states(): pl.pallas_call(kernel, out_shape=states_shape(plan.plane, plan.each), in_...  2.03 us
  transfers between devices with their start and end apart: 26, of which 5 were waited for; matrix products, arithmetic and copies ran while one was open for 0% of the time, Pallas kernels for 28%

profile of v13, /device:TPU:0, one launch (start us, length us, event | category | flops | bytes accessed | tf_op | source)
XLA Modules:
  0.0 68.2 jit_solution(11601040614711899488)
XLA Ops:
  0.6 0.1 pad_add_fusion.place_ref
  0.7 4.4 %decode.1 = (bf16[256,1024]{1,0:T(8,128)(2,1)S(1)}, bf16[256,1024]{1,0:T(8,128)(2,1)S(1)}, bf16[256,1024]{1,0:T(8,128)(2,1)S(1)}, bf16[256,1024]{1,0:T(8,128)(2,...) custom-call(s32[4]{0:T(128)S(1)} %pad_add_fusion.place_ref, ...), custom_call_target="tpu_custom_call" | custom-call | flops 4194304 | bytes 14680064 | tf_op jit(solution)/shard_map/decode/pallas_call | solution.py:106
  5.1 0.5 collective-permute-start.3
  5.6 0.1 collective-permute-start.4
  5.7 0.8 %spike_queries.1 = (bf16[256,1024]{1,0:T(8,128)(2,1)S(1)}, bf16[256,1024]{1,0:T(8,128)(2,1)S(1)}, bf16[256,1024]{1,0:T(8,128)(2,1)S(1)}, bf16[256,1024]{1,0:T(8,128)(2,1)S(1)}) custom-call(s32[4]{0:T(128)S(1)} %pad_add_fusion.place_ref, bf16[256,4096]{1,0:T(8,128)(2,1)S(1)} %copy-done, bf16[256,1024]{1,0:T(8,128)(2,1)S(1)} %get-tuple-element.36.refs_0_, ...), custom_call_target="tpu_custom_call" | custom-call | flops 1048576 | bytes 6291456 | tf_op jit(solution)/shard_map/spike_queries/pallas_call | solution.py:131
  6.5 0.5 collective-permute-start
  7.0 0.1 collective-permute-start.5
  7.1 0.4 collective-permute-start.1
  7.5 0.0 collective-permute-done.3.k_sib_ref.refs_3_
  7.5 0.1 collective-permute-start.2
  7.6 1.0 %core_states_0.1.refs_0_.mine_ref = f32[4,2,128,128]{3,2,1,0:T(8,128)S(1)} custom-call(s32[4]{0:T(128)S(1)} %pad_add_fusion.place_ref, bf16[256,1024]{1,0:T(8,128)(2,1)S(1)} %get-tuple-element.46.k_ref.refs_2_, bf16[256,1024]{1,0:T(8,128)(2,1)S(1)} %get-tuple-element.47.v_ref.refs_4_, bf16[256,1024]{1,0:T(8,128)(2,1)S(1)} %get-tuple-element.48.refs_0_.q_ref), custom_call_target="tpu_custom_call" | custom-call | flops 67108864 | bytes 1572864 | tf_op jit(solution)/shard_map/core_states_0/pallas_call | solution.py:228
  8.6 0.0 collective-permute-done.4.v_sib_ref.refs_5_
  8.7 1.0 %chunk_states_0.1 = (f32[2,128,128]{2,1,0:T(8,128)S(1)}, f32[4,2,128,128]{3,2,1,0:T(8,128)S(1)}, s16[288,128]{1,0:T(8,128)(2,1)S(1)}, s16[272,128]{1,0:T(8,128)(2,1)S(1)}, s16[272,128]{1,0:T(8,128)(2,1)S(1)}) custom-call(s32[4]{0:T(128)S(1)} %pad_add_fusion.place_ref, f32[4,2,128,128]{3,2,1,0:T(8,128)S(1)} %core_states_0.1.refs_0_.mine_ref, ...), custom_call_target="tpu_custom_call" | custom-call | flops 67108864 | bytes 2359296 | tf_op jit(solution)/shard_map/chunk_states_0/pallas_call | solution.py:262
  9.7 3.0 %collective-permute-start.6 = (s16[288,128]{1,0:T(8,128)(2,1)S(1)}, s16[288,128]{1,0:T(8,128)(2,1)S(1)}, u32[]{:S(2)}, u32[]{:S(2)}) collective-permute-start(s16[288,128]{1,0:T(8,128)(2,1)S(1)} %get-tuple-element.54), channel_id=1, source_target_pairs={{0,2},{2,0},{4,6},{6,4},{1,3},{3,1},{5,7},{7,5},{8,10},{10,8},{12,... | collective-permute-start | bytes 221192 | tf_op jit(solution)/shard_map/ppermute | solution.py:529
  12.7 1.4 %collective-permute-start.10 = (s16[272,128]{1,0:T(8,128)(2,1)S(1)}, s16[272,128]{1,0:T(8,128)(2,1)S(1)}, u32[]{:S(2)}, u32[]{:S(2)}) collective-permute-start(s16[272,128]{1,0:T(8,128)(2,1)S(1)} %get-tuple-element.59), channel_id=1, source_target_pairs={{0,6},{2,4},{4,2},{6,0},{1,7},{3,5},{5,3},{7,1},{8,14},{10,12},{12... | collective-permute-start | bytes 208904 | tf_op jit(solution)/shard_map/ppermute | solution.py:529
  14.2 0.0 collective-permute-done.5.refs_1_.refs_4_.q_sib_ref
  14.2 0.1 collective-permute-start.11
  14.3 1.0 %core_states_1.1.mine_ref = f32[4,2,128,128]{3,2,1,0:T(8,128)S(1)} custom-call(s32[4]{0:T(128)S(1)} %pad_add_fusion.place_ref, bf16[256,1024]{1,0:T(8,128)(2,1)S(1)} %get-tuple-element.42.k_ref.refs_2_, bf16[256,1024]{1,0:T(8,128)(2,1)S(1)} %get-tuple-element.44.v_ref.refs_4_, f32[4,2,128,128]{3,2,1,0:T(8,128)S(1)} %core_states_0.1.refs_0_.mine_ref), custom_call_target="tpu_custom_call" | custom-call | flops 67108864 | bytes 1572864 | tf_op jit(solution)/shard_map/core_states_1/pallas_call | solution.py:228
  15.3 0.0 collective-permute-done.2.v_sib_ref.refs_5_
  15.3 1.0 %chunk_states_1.1 = (f32[2,128,128]{2,1,0:T(8,128)S(1)}, f32[4,2,128,128]{3,2,1,0:T(8,128)S(1)}, s16[272,128]{1,0:T(8,128)(2,1)S(1)}, s16[272,128]{1,0:T(8,128)(2,1)S(1)}, s16[272,128]{1,0:T(8,128)(2,1)S(1)}) custom-call(s32[4]{0:T(128)S(1)} %pad_add_fusion.place_ref, f32[4,2,128,128]{3,2,1,0:T(8,128)S(1)} %core_states_1.1.mine_ref, ...), custom_call_target="tpu_custom_call" | custom-call | flops 67108864 | bytes 2359296 | tf_op jit(solution)/shard_map/chunk_states_1/pallas_call | solution.py:262
  16.4 2.0 %collective-permute-start.7 = (s16[272,128]{1,0:T(8,128)(2,1)S(1)}, s16[272,128]{1,0:T(8,128)(2,1)S(1)}, u32[]{:S(2)}, u32[]{:S(2)}) collective-permute-start(s16[272,128]{1,0:T(8,128)(2,1)S(1)} %get-tuple-element.56), channel_id=1, source_target_pairs={{0,2},{2,0},{4,6},{6,4},{1,3},{3,1},{5,7},{7,5},{8,10},{10,8},{12,... | collective-permute-start | bytes 208904 | tf_op jit(solution)/shard_map/ppermute | solution.py:529
  18.4 1.5 %collective-permute-start.8 = (s16[272,128]{1,0:T(8,128)(2,1)S(1)}, s16[272,128]{1,0:T(8,128)(2,1)S(1)}, u32[]{:S(2)}, u32[]{:S(2)}) collective-permute-start(s16[272,128]{1,0:T(8,128)(2,1)S(1)} %get-tuple-element.57), channel_id=1, source_target_pairs={{0,4},{2,6},{4,0},{6,2},{1,5},{3,7},{5,1},{7,3},{8,12},{10,14},{12... | collective-permute-start | bytes 208904 | tf_op jit(solution)/shard_map/ppermute | solution.py:529
  19.9 0.1 collective-permute-start.9
  19.9 0.0 collective-permute-done.11.refs_1_.refs_2_
  20.0 0.0 collective-permute-done.6.refs_2_.refs_0_.refs_4_.refs_7_.refs_1_
  20.0 0.1 level_states_0.1.refs_3_
  20.1 5.9 %collective-permute-start.17 = (s16[272,128]{1,0:T(8,128)(2,1)S(1)}, s16[272,128]{1,0:T(8,128)(2,1)S(1)}, u32[]{:S(2)}, u32[]{:S(2)}) collective-permute-start(s16[272,128]{1,0:T(8,128)(2,1)S(1)} %level_states_0.1.refs_3_), channel_id=1, source_target_pairs={{0,24},{1,25},{2,26},{3,27},{4,28},{5,29},{6,30},{7,31}} | collective-permute-start | bytes 208904 | tf_op jit(solution)/shard_map/ppermute | solution.py:536
  26.0 1.3 %collective-permute-start.16 = (s16[272,128]{1,0:T(8,128)(2,1)S(1)}, s16[272,128]{1,0:T(8,128)(2,1)S(1)}, u32[]{:S(2)}, u32[]{:S(2)}) collective-permute-start(s16[272,128]{1,0:T(8,128)(2,1)S(1)} %level_states_0.1.refs_3_), channel_id=1, source_target_pairs={{0,16},{8,24},{1,17},{9,25},{2,18},{10,26},{3,19},{11,27},{4,20},{... | collective-permute-start | bytes 208904 | tf_op jit(solution)/shard_map/ppermute | solution.py:536
  27.3 2.5 %collective-permute-start.15 = (s16[272,128]{1,0:T(8,128)(2,1)S(1)}, s16[272,128]{1,0:T(8,128)(2,1)S(1)}, u32[]{:S(2)}, u32[]{:S(2)}) collective-permute-start(s16[272,128]{1,0:T(8,128)(2,1)S(1)} %level_states_0.1.refs_3_), channel_id=1, source_target_pairs={{0,8},{8,16},{16,24},{1,9},{9,17},{17,25},{2,10},{10,18},{18,26},{... | collective-permute-start | bytes 208904 | tf_op jit(solution)/shard_map/ppermute | solution.py:536
  29.8 0.0 collective-permute-done.9.refs_0_.refs_2_.refs_10_
  29.8 0.1 level_states_1.1.refs_6_
  29.9 1.3 %collective-permute-start.14 = (s16[272,128]{1,0:T(8,128)(2,1)S(1)}, s16[272,128]{1,0:T(8,128)(2,1)S(1)}, u32[]{:S(2)}, u32[]{:S(2)}) collective-permute-start(s16[272,128]{1,0:T(8,128)(2,1)S(1)} %level_states_1.1.refs_6_), channel_id=1, source_target_pairs={{0,24},{1,25},{2,26},{3,27},{4,28},{5,29},{6,30},{7,31}} | collective-permute-start | bytes 208904 | tf_op jit(solution)/shard_map/ppermute | solution.py:536
  31.2 1.3 %collective-permute-start.13 = (s16[272,128]{1,0:T(8,128)(2,1)S(1)}, s16[272,128]{1,0:T(8,128)(2,1)S(1)}, u32[]{:S(2)}, u32[]{:S(2)}) collective-permute-start(s16[272,128]{1,0:T(8,128)(2,1)S(1)} %level_states_1.1.refs_6_), channel_id=1, source_target_pairs={{0,16},{8,24},{1,17},{9,25},{2,18},{10,26},{3,19},{11,27},{4,20},{... | collective-permute-start | bytes 208904 | tf_op jit(solution)/shard_map/ppermute | solution.py:536
  32.5 2.0 %collective-permute-start.12 = (s16[272,128]{1,0:T(8,128)(2,1)S(1)}, s16[272,128]{1,0:T(8,128)(2,1)S(1)}, u32[]{:S(2)}, u32[]{:S(2)}) collective-permute-start(s16[272,128]{1,0:T(8,128)(2,1)S(1)} %level_states_1.1.refs_6_), channel_id=1, source_target_pairs={{0,8},{8,16},{16,24},{1,9},{9,17},{17,25},{2,10},{10,18},{18,26},{... | collective-permute-start | bytes 208904 | tf_op jit(solution)/shard_map/ppermute | solution.py:536
  34.5 0.0 collective-permute-done.15.refs_3_.refs_4_
  34.5 0.8 %carries_0.1 = (s16[272,128]{1,0:T(8,128)(2,1)S(1)}, s16[272,128]{1,0:T(8,128)(2,1)S(1)}) custom-call(s32[4]{0:T(128)S(1)} %pad_add_fusion.place_ref, f32[2,128,128]{2,1,0:T(8,128)S(1)} %get-tuple-element.51.refs_0_.own_ref, s16[288,128]{1,0:T(8,128)(2,1)S(1)} %collective-permute-done.6.refs_2_.refs_0_.refs_4_.refs_7_.refs_1_, ...), custom_call_target="tpu_custom_call" | custom-call | bytes 1245184 | tf_op jit(solution)/shard_map/carries_0/pallas_call | solution.py:324
  35.3 1.8 %collective-permute-start.21 = (s16[272,128]{1,0:T(8,128)(2,1)S(1)}, s16[272,128]{1,0:T(8,128)(2,1)S(1)}, u32[]{:S(2)}, u32[]{:S(2)}) collective-permute-start(s16[272,128]{1,0:T(8,128)(2,1)S(1)} %get-tuple-element.65), channel_id=1, source_target_pairs={{0,6},{2,4},{4,2},{6,0},{1,7},{3,5},{5,3},{7,1},{8,14},{10,12},{12... | collective-permute-start | bytes 208904 | tf_op jit(solution)/shard_map/ppermute | solution.py:529
  37.1 0.5 collective-permute-start.20
  37.6 1.5 %attend_local_0_1_3.1.refs_6_.refs_2_ = f32[2,256,512]{2,1,0:T(8,128)S(1)} custom-call(s32[4]{0:T(128)S(1)} %pad_add_fusion.place_ref, bf16[256,1024]{1,0:T(8,128)(2,1)S(1)} %get-tuple-element.48.refs_0_.q_ref, bf16[256,1024]{1,0:T(8,128)(2,1)S(1)} %collective-permute-done.5.refs_1_.refs_4_.q_sib_ref, bf16[256,1024]{1,0:T(8,128)(2,1)S(1)} %get-tuple-element.46.k_ref.refs_2_, ...), custom_call_target="tpu_custom_call" | custom-call | flops 268435456 | bytes 2097152 | tf_op jit(solution)/shard_map/attend_local_0_1_3/pallas_call | solution.py:382
  39.1 0.0 collective-permute-done.14.refs_5_.refs_13_
  39.1 0.0 collective-permute-done.12.refs_3_.refs_11_
  39.1 0.8 %carries_1.1 = (s16[272,128]{1,0:T(8,128)(2,1)S(1)}, s16[272,128]{1,0:T(8,128)(2,1)S(1)}) custom-call(s32[4]{0:T(128)S(1)} %pad_add_fusion.place_ref, f32[2,128,128]{2,1,0:T(8,128)S(1)} %get-tuple-element.55.refs_3_.own_ref.refs_7_, s16[272,128]{1,0:T(8,128)(2,1)S(1)} %collective-permute-done.7.refs_2_.refs_0_.refs_8_, ...), custom_call_target="tpu_custom_call" | custom-call | bytes 1245184 | tf_op jit(solution)/shard_map/carries_1/pallas_call | solution.py:324
  39.9 1.6 %collective-permute-start.19 = (s16[272,128]{1,0:T(8,128)(2,1)S(1)}, s16[272,128]{1,0:T(8,128)(2,1)S(1)}, u32[]{:S(2)}, u32[]{:S(2)}) collective-permute-start(s16[272,128]{1,0:T(8,128)(2,1)S(1)} %get-tuple-element.63), channel_id=1, source_target_pairs={{0,6},{2,4},{4,2},{6,0},{1,7},{3,5},{5,3},{7,1},{8,14},{10,12},{12... | collective-permute-start | bytes 208904 | tf_op jit(solution)/shard_map/ppermute | solution.py:529
  41.4 1.2 %collective-permute-start.18 = (s16[272,128]{1,0:T(8,128)(2,1)S(1)}, s16[272,128]{1,0:T(8,128)(2,1)S(1)}, u32[]{:S(2)}, u32[]{:S(2)}) collective-permute-start(s16[272,128]{1,0:T(8,128)(2,1)S(1)} %get-tuple-element.62.refs_7_), channel_id=1, source_target_pairs={{0,2},{2,0},{4,6},{6,4},{1,3},{3,1},{5,7},{7,5},{8,10},{10,8},{12,... | collective-permute-start | bytes 208904 | tf_op jit(solution)/shard_map/ppermute | solution.py:529
  42.6 0.0 collective-permute-done.21.refs_6_
  42.6 0.1 collective-permute-done.20.refs_5_
  42.8 1.2 %attend_0_1_3.1.refs_10_ = bf16[512,512]{1,0:T(8,128)(2,1)S(1)} custom-call(s32[4]{0:T(128)S(1)} %pad_add_fusion.place_ref, bf16[256,1024]{1,0:T(8,128)(2,1)S(1)} %get-tuple-element.48.refs_0_.q_ref, bf16[256,1024]{1,0:T(8,128)(2,1)S(1)} %collective-permute-done.5.refs_1_.refs_4_.q_sib_ref, f32[2,256,512]{2,1,0:T(8,128)S(1)} %attend_local_0_1_3.1.refs_6_.refs_2_, ...), custom_call_target="tpu_custom_call" | custom-call | flops 402653184 | bytes 2097152 | tf_op jit(solution)/shard_map/attend_0_1_3/pallas_call | solution.py:454
  44.0 0.8 %collective-permute-start.24 = (bf16[512,512]{1,0:T(8,128)(2,1)S(1)}, bf16[512,512]{1,0:T(8,128)(2,1)S(1)}, u32[]{:S(2)}, u32[]{:S(2)}) collective-permute-start(bf16[512,512]{1,0:T(8,128)(2,1)S(1)} %attend_0_1_3.1.refs_10_), channel_id=1, source_target_pairs={{0,2},{2,0},{1,3},{3,1},{4,6},{6,4},{5,7},{7,5},{8,10},{10,8},{9,1... | collective-permute-start | bytes 1572872 | tf_op jit(solution)/shard_map/ppermute | solution.py:529
  44.7 0.6 collective-permute-done.19.refs_9_
  45.3 1.5 %collective-permute-done.18.refs_8_ = s16[272,128]{1,0:T(8,128)(2,1)S(1)} collective-permute-done((s16[272,128]{1,0:T(8,128)(2,1)S(1)}, s16[272,128]{1,0:T(8,128)(2,1)S(1)}, u32[]{:S(2)}, u32[]{:S(2)}) %collective-permute-start.18) | collective-permute-done | bytes 69664 | tf_op jit(solution)/shard_map/ppermute | solution.py:529
  46.8 1.9 %attend_1_1_3.1.refs_14_.refs_10_ = bf16[512,512]{1,0:T(8,128)(2,1)S(1)} custom-call(s32[4]{0:T(128)S(1)} %pad_add_fusion.place_ref, bf16[256,1024]{1,0:T(8,128)(2,1)S(1)} %get-tuple-element.40.refs_0_, bf16[256,1024]{1,0:T(8,128)(2,1)S(1)} %collective-permute-done.refs_2_.refs_5_.refs_1_, bf16[256,1024]{1,0:T(8,128)(2,1)S(1)} %get-tuple-element.42.k_ref.refs_2_, ...), custom_call_target="tpu_custom_call" | custom-call | flops 402653184 | bytes 2097152 | tf_op jit(solution)/shard_map/attend_1_1_3/pallas_call | solution.py:454
  48.7 1.6 %collective-permute-start.22 = (bf16[512,512]{1,0:T(8,128)(2,1)S(1)}, bf16[512,512]{1,0:T(8,128)(2,1)S(1)}, u32[]{:S(2)}, u32[]{:S(2)}) collective-permute-start(bf16[512,512]{1,0:T(8,128)(2,1)S(1)} %attend_1_1_3.1.refs_14_.refs_10_), channel_id=1, source_target_pairs={{0,2},{2,0},{1,3},{3,1},{4,6},{6,4},{5,7},{7,5},{8,10},{10,8},{9,1... | collective-permute-start | bytes 1572872 | tf_op jit(solution)/shard_map/ppermute | solution.py:529
  50.3 1.1 %own_carries.1 = (s16[528,128]{1,0:T(8,128)(2,1)S(1)}, s16[528,128]{1,0:T(8,128)(2,1)S(1)}, f32[2,2,128,128]{3,2,1,0:T(8,128)S(1)}, f32[2,2,128,128]{3,2,1,0:T(8,128)S(1)}) custom-call(s32[4]{0:T(128)S(1)} %pad_add_fusion.place_ref, f32[2,128,128]{2,1,0:T(8,128)S(1)} %get-tuple-element.51.refs_0_.own_ref, ...), custom_call_target="tpu_custom_call" | custom-call | bytes 2621440 | tf_op jit(solution)/shard_map/own_carries/pallas_call | solution.py:358
  51.4 0.6 collective-permute-start.25
  52.0 1.5 %collective-permute-start.23 = (s16[528,128]{1,0:T(8,128)(2,1)S(1)}, s16[528,128]{1,0:T(8,128)(2,1)S(1)}, u32[]{:S(2)}, u32[]{:S(2)}) collective-permute-start(s16[528,128]{1,0:T(8,128)(2,1)S(1)} %get-tuple-element.67), channel_id=1, source_target_pairs={{0,4},{2,6},{4,0},{6,2},{1,5},{3,7},{5,1},{7,3},{8,12},{10,14},{12... | collective-permute-start | bytes 405512 | tf_op jit(solution)/shard_map/ppermute | solution.py:529
  53.5 5.8 %collective-permute-done.23.refs_9_ = s16[528,128]{1,0:T(8,128)(2,1)S(1)} collective-permute-done((s16[528,128]{1,0:T(8,128)(2,1)S(1)}, s16[528,128]{1,0:T(8,128)(2,1)S(1)}, u32[]{:S(2)}, u32[]{:S(2)}) %collective-permute-start.23) | collective-permute-done | bytes 135200 | tf_op jit(solution)/shard_map/ppermute | solution.py:529
  59.3 1.9 %attend_0_0_2.1.refs_10_.refs_0_ = bf16[512,512]{1,0:T(8,128)(2,1)S(1)} custom-call(s32[4]{0:T(128)S(1)} %pad_add_fusion.place_ref, bf16[256,1024]{1,0:T(8,128)(2,1)S(1)} %get-tuple-element.48.refs_0_.q_ref, bf16[256,1024]{1,0:T(8,128)(2,1)S(1)} %collective-permute-done.5.refs_1_.refs_4_.q_sib_ref, bf16[256,1024]{1,0:T(8,128)(2,1)S(1)} %get-tuple-element.46.k_ref.refs_2_, ...), custom_call_target="tpu_custom_call" | custom-call | flops 402653184 | bytes 2097152 | tf_op jit(solution)/shard_map/attend_0_0_2/pallas_call | solution.py:454
  61.2 1.9 %attend_1_0_2.1.refs_1_ = bf16[512,512]{1,0:T(8,128)(2,1)S(1)} custom-call(s32[4]{0:T(128)S(1)} %pad_add_fusion.place_ref, bf16[256,1024]{1,0:T(8,128)(2,1)S(1)} %get-tuple-element.40.refs_0_, bf16[256,1024]{1,0:T(8,128)(2,1)S(1)} %collective-permute-done.refs_2_.refs_5_.refs_1_, bf16[256,1024]{1,0:T(8,128)(2,1)S(1)} %get-tuple-element.42.k_ref.refs_2_, ...), custom_call_target="tpu_custom_call" | custom-call | flops 402653184 | bytes 2097152 | tf_op jit(solution)/shard_map/attend_1_0_2/pallas_call | solution.py:454
  63.0 0.0 collective-permute-done.25.refs_1_
  63.1 1.4 %assemble_cache.1 = f32[1,8,128,128]{3,2,1,0:T(8,128)} custom-call(s32[4]{0:T(128)S(1)} %pad_add_fusion.place_ref, f32[2,2,128,128]{3,2,1,0:T(8,128)S(1)} %get-tuple-element.68.refs_0_, f32[2,2,128,128]{3,2,1,0:T(8,128)S(1)} %collective-permute-done.25.refs_1_), custom_call_target="tpu_custom_call" | custom-call | tf_op jit(solution)/shard_map/assemble_cache/pallas_call | solution.py:514
  64.4 0.0 collective-permute-done.24.refs_2_
  64.4 1.7 %assemble.1.refs_1_ = bf16[1024,1024]{1,0:T(8,128)(2,1)} custom-call(s32[4]{0:T(128)S(1)} %pad_add_fusion.place_ref, bf16[512,512]{1,0:T(8,128)(2,1)S(1)} %attend_0_0_2.1.refs_10_.refs_0_, bf16[512,512]{1,0:T(8,128)(2,1)S(1)} %attend_1_0_2.1.refs_1_, bf16[512,512]{1,0:T(8,128)(2,1)S(1)} %collective-permute-done.24.refs_2_), custom_call_target="tpu_custom_call" | custom-call | tf_op jit(solution)/shard_map/assemble/pallas_call | solution.py:493
  66.2 0.7 %collective-permute-done.22.refs_0_ = bf16[512,512]{1,0:T(8,128)(2,1)S(1)} collective-permute-done((bf16[512,512]{1,0:T(8,128)(2,1)S(1)}, bf16[512,512]{1,0:T(8,128)(2,1)S(1)}, u32[]{:S(2)}, u32[]{:S(2)}) %collective-permute-start.22) | collective-permute-done | bytes 524320 | tf_op jit(solution)/shard_map/ppermute | solution.py:529
  66.9 1.4 %finish.1 = bf16[1024,1024]{1,0:T(8,128)(2,1)} custom-call(s32[4]{0:T(128)S(1)} %pad_add_fusion.place_ref, bf16[512,512]{1,0:T(8,128)(2,1)S(1)} %collective-permute-done.22.refs_0_, bf16[1024,1024]{1,0:T(8,128)(2,1)} %assemble.1.refs_1_), custom_call_target="tpu_custom_call", output_to_operand_aliasing={{}: (2, {})} | custom-call | tf_op jit(solution)/shard_map/finish/pallas_call | solution.py:493
  (12 shorter events, 0.0 us)
Async XLA Ops:
  0.7 5.0 %copy-start = (bf16[256,4096]{1,0:T(8,128)(2,1)S(1)}, bf16[256,4096]{1,0:T(8,128)(2,1)}, u32[]{:S(2)}) copy-start(bf16[256,4096]{1,0:T(8,128)(2,1)} %queries_ref.1) | copy-start | bytes 6291460
  5.1 2.4 %collective-permute-start.3 = (bf16[256,1024]{1,0:T(8,128)(2,1)S(1)}, bf16[256,1024]{1,0:T(8,128)(2,1)S(1)}, u32[]{:S(2)}, u32[]{:S(2)}) collective-permute-start(bf16[256,1024]{1,0:T(8,128)(2,1)S(1)} %get-tuple-element.49), channel_id=1, source_target_pairs={{0,1},{1,0},{2,3},{3,2},{4,5},{5,4},{6,7},{7,6},{8,9},{9,8},{10,11... | collective-permute-start | bytes 1572872 | tf_op jit(solution)/shard_map/ppermute | solution.py:529
  5.6 3.0 %collective-permute-start.4 = (bf16[256,1024]{1,0:T(8,128)(2,1)S(1)}, bf16[256,1024]{1,0:T(8,128)(2,1)S(1)}, u32[]{:S(2)}, u32[]{:S(2)}) collective-permute-start(bf16[256,1024]{1,0:T(8,128)(2,1)S(1)} %get-tuple-element.50), channel_id=1, source_target_pairs={{0,1},{1,0},{2,3},{3,2},{4,5},{5,4},{6,7},{7,6},{8,9},{9,8},{10,11... | collective-permute-start | bytes 1572872 | tf_op jit(solution)/shard_map/ppermute | solution.py:529
  6.5 2.1 %copy-start.1 = (f32[1024]{0:T(1024)S(1)}, f32[1024]{0:T(1024)}, u32[]{:S(2)}) copy-start(f32[1024]{0:T(1024)} %param.9) | copy-start | bytes 12292
  6.5 6.2 %collective-permute-start = (bf16[256,1024]{1,0:T(8,128)(2,1)S(1)}, bf16[256,1024]{1,0:T(8,128)(2,1)S(1)}, u32[]{:S(2)}, u32[]{:S(2)}) collective-permute-start(bf16[256,1024]{1,0:T(8,128)(2,1)S(1)} %get-tuple-element.41), channel_id=1, source_target_pairs={{0,1},{1,0},{2,3},{3,2},{4,5},{5,4},{6,7},{7,6},{8,9},{9,8},{10,11... | collective-permute-start | bytes 1572872 | tf_op jit(solution)/shard_map/ppermute | solution.py:529
  7.0 7.1 %collective-permute-start.5 = (bf16[256,1024]{1,0:T(8,128)(2,1)S(1)}, bf16[256,1024]{1,0:T(8,128)(2,1)S(1)}, u32[]{:S(2)}, u32[]{:S(2)}) collective-permute-start(bf16[256,1024]{1,0:T(8,128)(2,1)S(1)} %get-tuple-element.52), channel_id=1, source_target_pairs={{0,1},{1,0},{2,3},{3,2},{4,5},{5,4},{6,7},{7,6},{8,9},{9,8},{10,11... | collective-permute-start | bytes 1572872 | tf_op jit(solution)/shard_map/ppermute | solution.py:529
  7.1 8.2 %collective-permute-start.1 = (bf16[256,1024]{1,0:T(8,128)(2,1)S(1)}, bf16[256,1024]{1,0:T(8,128)(2,1)S(1)}, u32[]{:S(2)}, u32[]{:S(2)}) collective-permute-start(bf16[256,1024]{1,0:T(8,128)(2,1)S(1)} %get-tuple-element.43), channel_id=1, source_target_pairs={{0,1},{1,0},{2,3},{3,2},{4,5},{5,4},{6,7},{7,6},{8,9},{9,8},{10,11... | collective-permute-start | bytes 1572872 | tf_op jit(solution)/shard_map/ppermute | solution.py:529
  7.5 7.8 %collective-permute-start.2 = (bf16[256,1024]{1,0:T(8,128)(2,1)S(1)}, bf16[256,1024]{1,0:T(8,128)(2,1)S(1)}, u32[]{:S(2)}, u32[]{:S(2)}) collective-permute-start(bf16[256,1024]{1,0:T(8,128)(2,1)S(1)} %get-tuple-element.45), channel_id=1, source_target_pairs={{0,1},{1,0},{2,3},{3,2},{4,5},{5,4},{6,7},{7,6},{8,9},{9,8},{10,11... | collective-permute-start | bytes 1572872 | tf_op jit(solution)/shard_map/ppermute | solution.py:529
  9.7 10.2 %collective-permute-start.6 = (s16[288,128]{1,0:T(8,128)(2,1)S(1)}, s16[288,128]{1,0:T(8,128)(2,1)S(1)}, u32[]{:S(2)}, u32[]{:S(2)}) collective-permute-start(s16[288,128]{1,0:T(8,128)(2,1)S(1)} %get-tuple-element.54), channel_id=1, source_target_pairs={{0,2},{2,0},{4,6},{6,4},{1,3},{3,1},{5,7},{7,5},{8,10},{10,8},{12,... | collective-permute-start | bytes 221192 | tf_op jit(solution)/shard_map/ppermute | solution.py:529
  12.7 7.2 %collective-permute-start.10 = (s16[272,128]{1,0:T(8,128)(2,1)S(1)}, s16[272,128]{1,0:T(8,128)(2,1)S(1)}, u32[]{:S(2)}, u32[]{:S(2)}) collective-permute-start(s16[272,128]{1,0:T(8,128)(2,1)S(1)} %get-tuple-element.59), channel_id=1, source_target_pairs={{0,6},{2,4},{4,2},{6,0},{1,7},{3,5},{5,3},{7,1},{8,14},{10,12},{12... | collective-permute-start | bytes 208904 | tf_op jit(solution)/shard_map/ppermute | solution.py:529
  14.2 5.8 %collective-permute-start.11 = (s16[272,128]{1,0:T(8,128)(2,1)S(1)}, s16[272,128]{1,0:T(8,128)(2,1)S(1)}, u32[]{:S(2)}, u32[]{:S(2)}) collective-permute-start(s16[272,128]{1,0:T(8,128)(2,1)S(1)} %get-tuple-element.60), channel_id=1, source_target_pairs={{0,4},{2,6},{4,0},{6,2},{1,5},{3,7},{5,1},{7,3},{8,12},{10,14},{12... | collective-permute-start | bytes 208904 | tf_op jit(solution)/shard_map/ppermute | solution.py:529
  16.4 10.9 %collective-permute-start.7 = (s16[272,128]{1,0:T(8,128)(2,1)S(1)}, s16[272,128]{1,0:T(8,128)(2,1)S(1)}, u32[]{:S(2)}, u32[]{:S(2)}) collective-permute-start(s16[272,128]{1,0:T(8,128)(2,1)S(1)} %get-tuple-element.56), channel_id=1, source_target_pairs={{0,2},{2,0},{4,6},{6,4},{1,3},{3,1},{5,7},{7,5},{8,10},{10,8},{12,... | collective-permute-start | bytes 208904 | tf_op jit(solution)/shard_map/ppermute | solution.py:529
  18.4 11.4 %collective-permute-start.8 = (s16[272,128]{1,0:T(8,128)(2,1)S(1)}, s16[272,128]{1,0:T(8,128)(2,1)S(1)}, u32[]{:S(2)}, u32[]{:S(2)}) collective-permute-start(s16[272,128]{1,0:T(8,128)(2,1)S(1)} %get-tuple-element.57), channel_id=1, source_target_pairs={{0,4},{2,6},{4,0},{6,2},{1,5},{3,7},{5,1},{7,3},{8,12},{10,14},{12... | collective-permute-start | bytes 208904 | tf_op jit(solution)/shard_map/ppermute | solution.py:529
  19.9 9.9 %collective-permute-start.9 = (s16[272,128]{1,0:T(8,128)(2,1)S(1)}, s16[272,128]{1,0:T(8,128)(2,1)S(1)}, u32[]{:S(2)}, u32[]{:S(2)}) collective-permute-start(s16[272,128]{1,0:T(8,128)(2,1)S(1)} %get-tuple-element.58), channel_id=1, source_target_pairs={{0,6},{2,4},{4,2},{6,0},{1,7},{3,5},{5,3},{7,1},{8,14},{10,12},{12... | collective-permute-start | bytes 208904 | tf_op jit(solution)/shard_map/ppermute | solution.py:529
  20.1 12.4 %collective-permute-start.17 = (s16[272,128]{1,0:T(8,128)(2,1)S(1)}, s16[272,128]{1,0:T(8,128)(2,1)S(1)}, u32[]{:S(2)}, u32[]{:S(2)}) collective-permute-start(s16[272,128]{1,0:T(8,128)(2,1)S(1)} %level_states_0.1.refs_3_), channel_id=1, source_target_pairs={{0,24},{1,25},{2,26},{3,27},{4,28},{5,29},{6,30},{7,31}} | collective-permute-start | bytes 208904 | tf_op jit(solution)/shard_map/ppermute | solution.py:536
  26.0 8.5 %collective-permute-start.16 = (s16[272,128]{1,0:T(8,128)(2,1)S(1)}, s16[272,128]{1,0:T(8,128)(2,1)S(1)}, u32[]{:S(2)}, u32[]{:S(2)}) collective-permute-start(s16[272,128]{1,0:T(8,128)(2,1)S(1)} %level_states_0.1.refs_3_), channel_id=1, source_target_pairs={{0,16},{8,24},{1,17},{9,25},{2,18},{10,26},{3,19},{11,27},{4,20},{... | collective-permute-start | bytes 208904 | tf_op jit(solution)/shard_map/ppermute | solution.py:536
  27.3 7.2 %collective-permute-start.15 = (s16[272,128]{1,0:T(8,128)(2,1)S(1)}, s16[272,128]{1,0:T(8,128)(2,1)S(1)}, u32[]{:S(2)}, u32[]{:S(2)}) collective-permute-start(s16[272,128]{1,0:T(8,128)(2,1)S(1)} %level_states_0.1.refs_3_), channel_id=1, source_target_pairs={{0,8},{8,16},{16,24},{1,9},{9,17},{17,25},{2,10},{10,18},{18,26},{... | collective-permute-start | bytes 208904 | tf_op jit(solution)/shard_map/ppermute | solution.py:536
  29.9 9.2 %collective-permute-start.14 = (s16[272,128]{1,0:T(8,128)(2,1)S(1)}, s16[272,128]{1,0:T(8,128)(2,1)S(1)}, u32[]{:S(2)}, u32[]{:S(2)}) collective-permute-start(s16[272,128]{1,0:T(8,128)(2,1)S(1)} %level_states_1.1.refs_6_), channel_id=1, source_target_pairs={{0,24},{1,25},{2,26},{3,27},{4,28},{5,29},{6,30},{7,31}} | collective-permute-start | bytes 208904 | tf_op jit(solution)/shard_map/ppermute | solution.py:536
  31.2 7.9 %collective-permute-start.13 = (s16[272,128]{1,0:T(8,128)(2,1)S(1)}, s16[272,128]{1,0:T(8,128)(2,1)S(1)}, u32[]{:S(2)}, u32[]{:S(2)}) collective-permute-start(s16[272,128]{1,0:T(8,128)(2,1)S(1)} %level_states_1.1.refs_6_), channel_id=1, source_target_pairs={{0,16},{8,24},{1,17},{9,25},{2,18},{10,26},{3,19},{11,27},{4,20},{... | collective-permute-start | bytes 208904 | tf_op jit(solution)/shard_map/ppermute | solution.py:536
  32.5 6.6 %collective-permute-start.12 = (s16[272,128]{1,0:T(8,128)(2,1)S(1)}, s16[272,128]{1,0:T(8,128)(2,1)S(1)}, u32[]{:S(2)}, u32[]{:S(2)}) collective-permute-start(s16[272,128]{1,0:T(8,128)(2,1)S(1)} %level_states_1.1.refs_6_), channel_id=1, source_target_pairs={{0,8},{8,16},{16,24},{1,9},{9,17},{17,25},{2,10},{10,18},{18,26},{... | collective-permute-start | bytes 208904 | tf_op jit(solution)/shard_map/ppermute | solution.py:536
  35.3 7.4 %collective-permute-start.21 = (s16[272,128]{1,0:T(8,128)(2,1)S(1)}, s16[272,128]{1,0:T(8,128)(2,1)S(1)}, u32[]{:S(2)}, u32[]{:S(2)}) collective-permute-start(s16[272,128]{1,0:T(8,128)(2,1)S(1)} %get-tuple-element.65), channel_id=1, source_target_pairs={{0,6},{2,4},{4,2},{6,0},{1,7},{3,5},{5,3},{7,1},{8,14},{10,12},{12... | collective-permute-start | bytes 208904 | tf_op jit(solution)/shard_map/ppermute | solution.py:529
  37.1 5.7 %collective-permute-start.20 = (s16[272,128]{1,0:T(8,128)(2,1)S(1)}, s16[272,128]{1,0:T(8,128)(2,1)S(1)}, u32[]{:S(2)}, u32[]{:S(2)}) collective-permute-start(s16[272,128]{1,0:T(8,128)(2,1)S(1)} %get-tuple-element.61.refs_0_), channel_id=1, source_target_pairs={{0,2},{2,0},{4,6},{6,4},{1,3},{3,1},{5,7},{7,5},{8,10},{10,8},{12,... | collective-permute-start | bytes 208904 | tf_op jit(solution)/shard_map/ppermute | solution.py:529
  39.9 5.4 %collective-permute-start.19 = (s16[272,128]{1,0:T(8,128)(2,1)S(1)}, s16[272,128]{1,0:T(8,128)(2,1)S(1)}, u32[]{:S(2)}, u32[]{:S(2)}) collective-permute-start(s16[272,128]{1,0:T(8,128)(2,1)S(1)} %get-tuple-element.63), channel_id=1, source_target_pairs={{0,6},{2,4},{4,2},{6,0},{1,7},{3,5},{5,3},{7,1},{8,14},{10,12},{12... | collective-permute-start | bytes 208904 | tf_op jit(solution)/shard_map/ppermute | solution.py:529
  41.4 5.4 %collective-permute-start.18 = (s16[272,128]{1,0:T(8,128)(2,1)S(1)}, s16[272,128]{1,0:T(8,128)(2,1)S(1)}, u32[]{:S(2)}, u32[]{:S(2)}) collective-permute-start(s16[272,128]{1,0:T(8,128)(2,1)S(1)} %get-tuple-element.62.refs_7_), channel_id=1, source_target_pairs={{0,2},{2,0},{4,6},{6,4},{1,3},{3,1},{5,7},{7,5},{8,10},{10,8},{12,... | collective-permute-start | bytes 208904 | tf_op jit(solution)/shard_map/ppermute | solution.py:529
  44.0 20.5 %collective-permute-start.24 = (bf16[512,512]{1,0:T(8,128)(2,1)S(1)}, bf16[512,512]{1,0:T(8,128)(2,1)S(1)}, u32[]{:S(2)}, u32[]{:S(2)}) collective-permute-start(bf16[512,512]{1,0:T(8,128)(2,1)S(1)} %attend_0_1_3.1.refs_10_), channel_id=1, source_target_pairs={{0,2},{2,0},{1,3},{3,1},{4,6},{6,4},{5,7},{7,5},{8,10},{10,8},{9,1... | collective-permute-start | bytes 1572872 | tf_op jit(solution)/shard_map/ppermute | solution.py:529
  48.7 18.2 %collective-permute-start.22 = (bf16[512,512]{1,0:T(8,128)(2,1)S(1)}, bf16[512,512]{1,0:T(8,128)(2,1)S(1)}, u32[]{:S(2)}, u32[]{:S(2)}) collective-permute-start(bf16[512,512]{1,0:T(8,128)(2,1)S(1)} %attend_1_1_3.1.refs_14_.refs_10_), channel_id=1, source_target_pairs={{0,2},{2,0},{1,3},{3,1},{4,6},{6,4},{5,7},{7,5},{8,10},{10,8},{9,1... | collective-permute-start | bytes 1572872 | tf_op jit(solution)/shard_map/ppermute | solution.py:529
  51.4 11.6 %collective-permute-start.25 = (f32[2,2,128,128]{3,2,1,0:T(8,128)S(1)}, f32[2,2,128,128]{3,2,1,0:T(8,128)S(1)}, u32[]{:S(2)}, u32[]{:S(2)}) collective-permute-start(f32[2,2,128,128]{3,2,1,0:T(8,128)S(1)} %get-tuple-element.69), channel_id=1, source_target_pairs={{0,4},{4,0},{1,5},{5,1},{2,6},{6,2},{3,7},{7,3},{8,12},{12,8},{9,1... | collective-permute-start | bytes 786440 | tf_op jit(solution)/shard_map/ppermute | solution.py:529
  52.0 7.3 %collective-permute-start.23 = (s16[528,128]{1,0:T(8,128)(2,1)S(1)}, s16[528,128]{1,0:T(8,128)(2,1)S(1)}, u32[]{:S(2)}, u32[]{:S(2)}) collective-permute-start(s16[528,128]{1,0:T(8,128)(2,1)S(1)} %get-tuple-element.67), channel_id=1, source_target_pairs={{0,4},{2,6},{4,0},{6,2},{1,5},{3,7},{5,1},{7,3},{8,12},{10,14},{12... | collective-permute-start | bytes 405512 | tf_op jit(solution)/shard_map/ppermute | solution.py:529

commit v14 on v13

--- a/solution.py
+++ b/solution.py
@@ -217,36 +217,17 @@
     return pl.ds(pl.multiple_of(start, HD), HD)
 
 
-def core_states(plan, place, key, value, half, after):
-    def kernel(place_ref, k_ref, v_ref, *refs):
-        for offset in range(plan.plane):
-            for i in range(plan.each):
-                at = owned_columns(plan, place_ref, offset, i)
-                refs[-1][offset, i] = contract_rows(v_ref[:, at], k_ref[:, at])
-
-    heads = plan.plane * plan.each
-    return pl.pallas_call(
-        kernel,
-        out_shape=states_shape(plan.plane, plan.each),
-        in_specs=[SMEM] + [VMEM] * 2 + [ANY] * len(after),
-        out_specs=VMEM,
-        compiler_params=params(),
-        cost_estimate=cost(2 * plan.rows * HD * HD * heads, 4 * heads * HD * (plan.rows + HD)),
-        name=f"core_states_{half}",
-    )(place, key, value, *after)
-
-
-def chunk_states(plan, place, mine, key_sib, value_sib, half, after, gain=None):
+def chunk_states(plan, place, key, value, half, after, gain=None):
     gains = [] if gain is None else [gain]
 
-    def kernel(place_ref, mine_ref, k_sib_ref, v_sib_ref, *refs):
+    def kernel(place_ref, k_ref, k_sib_ref, v_ref, v_sib_ref, *refs):
         own_ref, first_ref, *send_refs = refs[len(gains) + len(after) :]
         is_first = jnp.full((HD, HD), place_ref[0], jnp.int32) == 0
         for offset in (*range(1, plan.plane), 0):
             states = []
             for i in range(plan.each):
                 at = owned_columns(plan, place_ref, offset, i)
-                mine = mine_ref[offset, i]
+                mine = contract_rows(v_ref[:, at], k_ref[:, at])
                 sib = contract_rows(v_sib_ref[:, at], k_sib_ref[:, at])
                 first_ref[offset, i] = jnp.where(is_first, mine, sib)
                 states.append(mine + sib)
@@ -266,14 +247,14 @@
             coded_shape(plan.each, PAD if gains and o < plan.n_y else 0)
             for o in range(1, plan.plane)
         ],
-        in_specs=[SMEM] + [VMEM] * (3 + len(gains)) + [ANY] * len(after),
+        in_specs=[SMEM] + [VMEM] * (4 + len(gains)) + [ANY] * len(after),
         out_specs=[VMEM] * (1 + plan.plane),
         compiler_params=params(),
         cost_estimate=cost(
-            2 * plan.rows * HD * HD * heads, 4 * plan.rows * HD * heads + 10 * heads * HD * HD
+            4 * plan.rows * HD * HD * heads, 8 * plan.rows * HD * heads + 6 * heads * HD * HD
         ),
         name=f"chunk_states_{half}",
-    )(place, mine, key_sib, value_sib, *gains, *after)
+    )(place, *key, *value, *gains, *after)
 
 
 def level_states(plan, own, others, half, after):
@@ -546,17 +527,12 @@
     spiked = spike_queries(plan, place, queries, [*parts[4], *parts[5]])
     query = with_siblings(spiked[: plan.halves], spiked[plan.halves :])
 
-    after = [query[0][0]]
-    of_core = []
-    for half in halves:
-        of_core.append(core_states(plan, place, key[half][0], value[half][0], half, after))
-        after = [of_core[half]]
     own, first, others = [], [], []
 
     def owner_stage(half, after):
         with_gain = gain if half == 0 else None
         mine, of_first, *sends = chunk_states(
-            plan, place, of_core[half], key[half][1], value[half][1], half, after, with_gain
+            plan, place, key[half], value[half], half, after, with_gain
         )
         own.append(mine)
         first.append(of_first)
@@ -594,7 +570,7 @@
             after = [part]
         return after
 
-    after = []
+    after = [query[0][0]]
     for half in halves:
         owner_stage(half, after)
         after = [own[-1], *[a for _, a in query]]
@@ -603,15 +579,15 @@
         level = level_states(plan, own[half], others[half][::-1], half, after)
         levels.append([to_later(level, d) for d in range(1, plan.n_outer)])
         after = [level]
-    carry, local = [], {}
+    local = {}
+    for y in range(1, plan.n_y):
+        local[y] = attend_local(plan, place, query[0], key[0], value[0], 0, of_group[y], after)
+        after = [local[y]]
+    carry = []
     for half in halves:
         done, of_half = carry_stage(half, after)
         carry.append(of_half)
         after = [done]
-        for y in range(1, plan.n_y):
-            if half == 0:
-                local[y] = attend_local(plan, place, query[0], key[0], value[0], 0, of_group[y], after)
-                after = [local[y]]
     for half in halves:
         after = send_stage(half, carry[half], after, {} if half else local)
     sends = own_carries(plan, place, own, others, levels, of_group[0], after)

time: 68.5 us -> 68.1 us (level)
  Pallas kernels: 24.8 us -> 23.4 us
  starting transfers between devices: 33.6 us -> 34.3 us
    pallas_call x2 -> x0, Pallas kernels: 2.03 us -> none  [core_states(): pl.pallas_call(kernel, out_shape=states_shape(plan.plane, plan.each), in_...]
    ppermute x20, starting transfers between devices: 19.3 us -> 20.5 us  [swap(): return lax.ppermute(array, axes, [(i, i ^ offset) for i in range(size)])]
  transfers between devices with their start and end apart: 26 -> 26, of which waited for: 5 -> 5; matrix products, arithmetic and copies ran while one was open for 0% -> 0% of each run, Pallas kernels for 28% -> 26%
where the time goes in v14:
time: 68.1 us; the launch traced here: 67.8 us
  starting transfers between devices  34.3 us (50%)
  Pallas kernels  23.4 us (34%)
  waiting for transfers between devices  9.22 us (14%)
  between operations  0.85 us (1%)
    ppermute x20, starting transfers between devices, swap(): return lax.ppermute(array, axes, [(i, i ^ offset) for i in range(size)])  20.5 us
    ppermute x6, starting transfers between devices, to_later(): return lax.ppermute(array, 'outer', pairs)  13.7 us
    ppermute x20, waiting for transfers between devices, swap(): return lax.ppermute(array, axes, [(i, i ^ offset) for i in range(size)])  9.2 us
    pallas_call x4, Pallas kernels, attend(): pl.pallas_call(kernel, out_shape=jax.ShapeDtypeStruct((CORES * rows, head...  6.78 us
    pallas_call x1, Pallas kernels, decode(): pl.pallas_call(kernel, out_shape=[jax.ShapeDtypeStruct((rows, plan.n_y *...  4.36 us
    pallas_call x2, Pallas kernels, assemble(): pl.pallas_call(kernel, out_shape=jax.ShapeDtypeStruct((plan.n_y * rows, p...  3.08 us
    pallas_call x2, Pallas kernels, chunk_states(): pl.pallas_call(kernel, out_shape=[states_shape(plan.each), states_shape(p...  2.73 us
    pallas_call x2, Pallas kernels, carries(): pl.pallas_call(kernel, out_shape=[coded_shape(plan.each)] * len(offsets),...  1.5 us
  transfers between devices with their start and end apart: 26, of which 5 were waited for; matrix products, arithmetic and copies ran while one was open for 0% of the time, Pallas kernels for 26%

profile of v14, /device:TPU:0, one launch (start us, length us, event | category | flops | bytes accessed | tf_op | source)
XLA Modules:
  0.0 67.8 jit_solution(13839886101630623665)
XLA Ops:
  0.6 0.1 pad_add_fusion.place_ref
  0.7 4.4 %decode.1 = (bf16[256,1024]{1,0:T(8,128)(2,1)S(1)}, bf16[256,1024]{1,0:T(8,128)(2,1)S(1)}, bf16[256,1024]{1,0:T(8,128)(2,1)S(1)}, bf16[256,1024]{1,0:T(8,128)(2,...) custom-call(s32[4]{0:T(128)S(1)} %pad_add_fusion.place_ref, ...), custom_call_target="tpu_custom_call" | custom-call | flops 4194304 | bytes 14680064 | tf_op jit(solution)/shard_map/decode/pallas_call | solution.py:106
  5.1 0.5 collective-permute-start.3
  5.6 0.1 collective-permute-start.4
  5.7 0.8 %spike_queries.1 = (bf16[256,1024]{1,0:T(8,128)(2,1)S(1)}, bf16[256,1024]{1,0:T(8,128)(2,1)S(1)}, bf16[256,1024]{1,0:T(8,128)(2,1)S(1)}, bf16[256,1024]{1,0:T(8,128)(2,1)S(1)}) custom-call(s32[4]{0:T(128)S(1)} %pad_add_fusion.place_ref, bf16[256,4096]{1,0:T(8,128)(2,1)S(1)} %copy-done, bf16[256,1024]{1,0:T(8,128)(2,1)S(1)} %get-tuple-element.36.refs_0_, ...), custom_call_target="tpu_custom_call" | custom-call | flops 1048576 | bytes 6291456 | tf_op jit(solution)/shard_map/spike_queries/pallas_call | solution.py:131
  6.5 0.5 collective-permute-start
  7.0 0.1 collective-permute-start.5
  7.1 0.4 collective-permute-start.1
  7.5 0.0 collective-permute-done.3.k_sib_ref.refs_3_
  7.5 0.1 collective-permute-start.2
  7.6 0.3 collective-permute-done.4.v_sib_ref.refs_5_
  7.9 1.4 %chunk_states_0.1 = (f32[2,128,128]{2,1,0:T(8,128)S(1)}, f32[4,2,128,128]{3,2,1,0:T(8,128)S(1)}, s16[288,128]{1,0:T(8,128)(2,1)S(1)}, s16[272,128]{1,0:T(8,128)(2,1)S(1)}, s16[272,128]{1,0:T(8,128)(2,1)S(1)}) custom-call(s32[4]{0:T(128)S(1)} %pad_add_fusion.place_ref, bf16[256,1024]{1,0:T(8,128)(2,1)S(1)} %get-tuple-element.46.k_ref.refs_2_, ...), custom_call_target="tpu_custom_call" | custom-call | flops 134217728 | bytes 2883584 | tf_op jit(solution)/shard_map/chunk_states_0/pallas_call | solution.py:243
  9.3 3.0 %collective-permute-start.6 = (s16[288,128]{1,0:T(8,128)(2,1)S(1)}, s16[288,128]{1,0:T(8,128)(2,1)S(1)}, u32[]{:S(2)}, u32[]{:S(2)}) collective-permute-start(s16[288,128]{1,0:T(8,128)(2,1)S(1)} %get-tuple-element.54), channel_id=1, source_target_pairs={{0,2},{2,0},{4,6},{6,4},{1,3},{3,1},{5,7},{7,5},{8,10},{10,8},{12,... | collective-permute-start | bytes 221192 | tf_op jit(solution)/shard_map/ppermute | solution.py:510
  12.2 0.0 collective-permute-done.refs_2_.refs_5_.refs_1_
  12.2 1.4 %collective-permute-start.10 = (s16[272,128]{1,0:T(8,128)(2,1)S(1)}, s16[272,128]{1,0:T(8,128)(2,1)S(1)}, u32[]{:S(2)}, u32[]{:S(2)}) collective-permute-start(s16[272,128]{1,0:T(8,128)(2,1)S(1)} %get-tuple-element.59), channel_id=1, source_target_pairs={{0,6},{2,4},{4,2},{6,0},{1,7},{3,5},{5,3},{7,1},{8,14},{10,12},{12... | collective-permute-start | bytes 208904 | tf_op jit(solution)/shard_map/ppermute | solution.py:510
  13.7 0.0 collective-permute-done.5.refs_1_.refs_4_.q_sib_ref
  13.7 0.1 collective-permute-start.11
  13.8 0.0 collective-permute-done.1.k_sib_ref.refs_3_
  13.8 0.0 collective-permute-done.2.v_sib_ref.refs_5_
  13.8 1.4 %chunk_states_1.1 = (f32[2,128,128]{2,1,0:T(8,128)S(1)}, f32[4,2,128,128]{3,2,1,0:T(8,128)S(1)}, s16[272,128]{1,0:T(8,128)(2,1)S(1)}, s16[272,128]{1,0:T(8,128)(2,1)S(1)}, s16[272,128]{1,0:T(8,128)(2,1)S(1)}) custom-call(s32[4]{0:T(128)S(1)} %pad_add_fusion.place_ref, bf16[256,1024]{1,0:T(8,128)(2,1)S(1)} %get-tuple-element.42.k_ref.refs_2_, ...), custom_call_target="tpu_custom_call" | custom-call | flops 134217728 | bytes 2883584 | tf_op jit(solution)/shard_map/chunk_states_1/pallas_call | solution.py:243
  15.2 2.0 %collective-permute-start.7 = (s16[272,128]{1,0:T(8,128)(2,1)S(1)}, s16[272,128]{1,0:T(8,128)(2,1)S(1)}, u32[]{:S(2)}, u32[]{:S(2)}) collective-permute-start(s16[272,128]{1,0:T(8,128)(2,1)S(1)} %get-tuple-element.56), channel_id=1, source_target_pairs={{0,2},{2,0},{4,6},{6,4},{1,3},{3,1},{5,7},{7,5},{8,10},{10,8},{12,... | collective-permute-start | bytes 208904 | tf_op jit(solution)/shard_map/ppermute | solution.py:510
  17.2 1.5 %collective-permute-start.8 = (s16[272,128]{1,0:T(8,128)(2,1)S(1)}, s16[272,128]{1,0:T(8,128)(2,1)S(1)}, u32[]{:S(2)}, u32[]{:S(2)}) collective-permute-start(s16[272,128]{1,0:T(8,128)(2,1)S(1)} %get-tuple-element.57), channel_id=1, source_target_pairs={{0,4},{2,6},{4,0},{6,2},{1,5},{3,7},{5,1},{7,3},{8,12},{10,14},{12... | collective-permute-start | bytes 208904 | tf_op jit(solution)/shard_map/ppermute | solution.py:510
  18.7 0.0 collective-permute-done.10.refs_0_.refs_2_.refs_3_
  18.7 0.6 collective-permute-start.9
  19.2 0.0 collective-permute-done.11.refs_1_.refs_2_
  19.2 0.0 collective-permute-done.6.refs_2_.refs_0_.refs_4_.refs_7_.refs_1_
  19.2 0.1 level_states_0.1.refs_3_
  19.4 5.5 %collective-permute-start.17 = (s16[272,128]{1,0:T(8,128)(2,1)S(1)}, s16[272,128]{1,0:T(8,128)(2,1)S(1)}, u32[]{:S(2)}, u32[]{:S(2)}) collective-permute-start(s16[272,128]{1,0:T(8,128)(2,1)S(1)} %level_states_0.1.refs_3_), channel_id=1, source_target_pairs={{0,24},{1,25},{2,26},{3,27},{4,28},{5,29},{6,30},{7,31}} | collective-permute-start | bytes 208904 | tf_op jit(solution)/shard_map/ppermute | solution.py:517
  24.9 1.3 %collective-permute-start.16 = (s16[272,128]{1,0:T(8,128)(2,1)S(1)}, s16[272,128]{1,0:T(8,128)(2,1)S(1)}, u32[]{:S(2)}, u32[]{:S(2)}) collective-permute-start(s16[272,128]{1,0:T(8,128)(2,1)S(1)} %level_states_0.1.refs_3_), channel_id=1, source_target_pairs={{0,16},{8,24},{1,17},{9,25},{2,18},{10,26},{3,19},{11,27},{4,20},{... | collective-permute-start | bytes 208904 | tf_op jit(solution)/shard_map/ppermute | solution.py:517
  26.2 0.0 collective-permute-done.7.refs_2_.refs_0_.refs_8_
  26.2 2.5 %collective-permute-start.15 = (s16[272,128]{1,0:T(8,128)(2,1)S(1)}, s16[272,128]{1,0:T(8,128)(2,1)S(1)}, u32[]{:S(2)}, u32[]{:S(2)}) collective-permute-start(s16[272,128]{1,0:T(8,128)(2,1)S(1)} %level_states_0.1.refs_3_), channel_id=1, source_target_pairs={{0,8},{8,16},{16,24},{1,9},{9,17},{17,25},{2,10},{10,18},{18,26},{... | collective-permute-start | bytes 208904 | tf_op jit(solution)/shard_map/ppermute | solution.py:517
  28.7 0.0 collective-permute-done.8.refs_1_.refs_9_
  28.7 0.1 level_states_1.1.refs_0_
  28.8 1.3 %collective-permute-start.14 = (s16[272,128]{1,0:T(8,128)(2,1)S(1)}, s16[272,128]{1,0:T(8,128)(2,1)S(1)}, u32[]{:S(2)}, u32[]{:S(2)}) collective-permute-start(s16[272,128]{1,0:T(8,128)(2,1)S(1)} %level_states_1.1.refs_0_), channel_id=1, source_target_pairs={{0,24},{1,25},{2,26},{3,27},{4,28},{5,29},{6,30},{7,31}} | collective-permute-start | bytes 208904 | tf_op jit(solution)/shard_map/ppermute | solution.py:517
  30.1 1.3 %collective-permute-start.13 = (s16[272,128]{1,0:T(8,128)(2,1)S(1)}, s16[272,128]{1,0:T(8,128)(2,1)S(1)}, u32[]{:S(2)}, u32[]{:S(2)}) collective-permute-start(s16[272,128]{1,0:T(8,128)(2,1)S(1)} %level_states_1.1.refs_0_), channel_id=1, source_target_pairs={{0,16},{8,24},{1,17},{9,25},{2,18},{10,26},{3,19},{11,27},{4,20},{... | collective-permute-start | bytes 208904 | tf_op jit(solution)/shard_map/ppermute | solution.py:517
  31.4 0.0 collective-permute-done.17.refs_5_.refs_6_
  31.4 1.9 %collective-permute-start.12 = (s16[272,128]{1,0:T(8,128)(2,1)S(1)}, s16[272,128]{1,0:T(8,128)(2,1)S(1)}, u32[]{:S(2)}, u32[]{:S(2)}) collective-permute-start(s16[272,128]{1,0:T(8,128)(2,1)S(1)} %level_states_1.1.refs_0_), channel_id=1, source_target_pairs={{0,8},{8,16},{16,24},{1,9},{9,17},{17,25},{2,10},{10,18},{18,26},{... | collective-permute-start | bytes 208904 | tf_op jit(solution)/shard_map/ppermute | solution.py:517
  33.3 1.5 %attend_local_0_1_3.1.refs_6_.refs_2_ = f32[2,256,512]{2,1,0:T(8,128)S(1)} custom-call(s32[4]{0:T(128)S(1)} %pad_add_fusion.place_ref, bf16[256,1024]{1,0:T(8,128)(2,1)S(1)} %get-tuple-element.50.refs_1_.q_ref.refs_0_, bf16[256,1024]{1,0:T(8,128)(2,1)S(1)} %collective-permute-done.5.refs_1_.refs_4_.q_sib_ref, ...), custom_call_target="tpu_custom_call" | custom-call | flops 268435456 | bytes 2097152 | tf_op jit(solution)/shard_map/attend_local_0_1_3/pallas_call | solution.py:363
  34.8 0.0 collective-permute-done.15.refs_3_.refs_4_
  34.8 0.8 %carries_0.1 = (s16[272,128]{1,0:T(8,128)(2,1)S(1)}, s16[272,128]{1,0:T(8,128)(2,1)S(1)}) custom-call(s32[4]{0:T(128)S(1)} %pad_add_fusion.place_ref, f32[2,128,128]{2,1,0:T(8,128)S(1)} %get-tuple-element.51.refs_0_.own_ref, s16[288,128]{1,0:T(8,128)(2,1)S(1)} %collective-permute-done.6.refs_2_.refs_0_.refs_4_.refs_7_.refs_1_, ...), custom_call_target="tpu_custom_call" | custom-call | bytes 1245184 | tf_op jit(solution)/shard_map/carries_0/pallas_call | solution.py:305
  35.5 1.8 %collective-permute-start.21 = (s16[272,128]{1,0:T(8,128)(2,1)S(1)}, s16[272,128]{1,0:T(8,128)(2,1)S(1)}, u32[]{:S(2)}, u32[]{:S(2)}) collective-permute-start(s16[272,128]{1,0:T(8,128)(2,1)S(1)} %get-tuple-element.65), channel_id=1, source_target_pairs={{0,6},{2,4},{4,2},{6,0},{1,7},{3,5},{5,3},{7,1},{8,14},{10,12},{12... | collective-permute-start | bytes 208904 | tf_op jit(solution)/shard_map/ppermute | solution.py:510
  37.4 0.5 collective-permute-start.20
  37.9 0.0 collective-permute-done.12.refs_3_.refs_11_
  37.9 0.8 %carries_1.1 = (s16[272,128]{1,0:T(8,128)(2,1)S(1)}, s16[272,128]{1,0:T(8,128)(2,1)S(1)}) custom-call(s32[4]{0:T(128)S(1)} %pad_add_fusion.place_ref, f32[2,128,128]{2,1,0:T(8,128)S(1)} %get-tuple-element.55.refs_3_.own_ref.refs_7_, s16[272,128]{1,0:T(8,128)(2,1)S(1)} %collective-permute-done.7.refs_2_.refs_0_.refs_8_, ...), custom_call_target="tpu_custom_call" | custom-call | bytes 1245184 | tf_op jit(solution)/shard_map/carries_1/pallas_call | solution.py:305
  38.7 1.7 %collective-permute-start.19 = (s16[272,128]{1,0:T(8,128)(2,1)S(1)}, s16[272,128]{1,0:T(8,128)(2,1)S(1)}, u32[]{:S(2)}, u32[]{:S(2)}) collective-permute-start(s16[272,128]{1,0:T(8,128)(2,1)S(1)} %get-tuple-element.63), channel_id=1, source_target_pairs={{0,6},{2,4},{4,2},{6,0},{1,7},{3,5},{5,3},{7,1},{8,14},{10,12},{12... | collective-permute-start | bytes 208904 | tf_op jit(solution)/shard_map/ppermute | solution.py:510
  40.3 1.1 %collective-permute-start.18 = (s16[272,128]{1,0:T(8,128)(2,1)S(1)}, s16[272,128]{1,0:T(8,128)(2,1)S(1)}, u32[]{:S(2)}, u32[]{:S(2)}) collective-permute-start(s16[272,128]{1,0:T(8,128)(2,1)S(1)} %get-tuple-element.62.refs_7_), channel_id=1, source_target_pairs={{0,2},{2,0},{4,6},{6,4},{1,3},{3,1},{5,7},{7,5},{8,10},{10,8},{12,... | collective-permute-start | bytes 208904 | tf_op jit(solution)/shard_map/ppermute | solution.py:510
  41.4 1.2 %collective-permute-done.20.refs_5_ = s16[272,128]{1,0:T(8,128)(2,1)S(1)} collective-permute-done((s16[272,128]{1,0:T(8,128)(2,1)S(1)}, s16[272,128]{1,0:T(8,128)(2,1)S(1)}, u32[]{:S(2)}, u32[]{:S(2)}) %collective-permute-start.20) | collective-permute-done | bytes 69664 | tf_op jit(solution)/shard_map/ppermute | solution.py:510
  42.6 1.2 %attend_0_1_3.1.refs_10_ = bf16[512,512]{1,0:T(8,128)(2,1)S(1)} custom-call(s32[4]{0:T(128)S(1)} %pad_add_fusion.place_ref, bf16[256,1024]{1,0:T(8,128)(2,1)S(1)} %get-tuple-element.50.refs_1_.q_ref.refs_0_, bf16[256,1024]{1,0:T(8,128)(2,1)S(1)} %collective-permute-done.5.refs_1_.refs_4_.q_sib_ref, f32[2,256,512]{2,1,0:T(8,128)S(1)} %attend_local_0_1_3.1.refs_6_.refs_2_, ...), custom_call_target="tpu_custom_call" | custom-call | flops 402653184 | bytes 2097152 | tf_op jit(solution)/shard_map/attend_0_1_3/pallas_call | solution.py:435
  43.8 1.5 %collective-permute-start.24 = (bf16[512,512]{1,0:T(8,128)(2,1)S(1)}, bf16[512,512]{1,0:T(8,128)(2,1)S(1)}, u32[]{:S(2)}, u32[]{:S(2)}) collective-permute-start(bf16[512,512]{1,0:T(8,128)(2,1)S(1)} %attend_0_1_3.1.refs_10_), channel_id=1, source_target_pairs={{0,2},{2,0},{1,3},{3,1},{4,6},{6,4},{5,7},{7,5},{8,10},{10,8},{9,1... | collective-permute-start | bytes 1572872 | tf_op jit(solution)/shard_map/ppermute | solution.py:510
  45.3 0.0 collective-permute-done.19.refs_9_
  45.3 0.3 collective-permute-done.18.refs_8_
  45.6 1.9 %attend_1_1_3.1.refs_14_.refs_10_ = bf16[512,512]{1,0:T(8,128)(2,1)S(1)} custom-call(s32[4]{0:T(128)S(1)} %pad_add_fusion.place_ref, bf16[256,1024]{1,0:T(8,128)(2,1)S(1)} %get-tuple-element.40.refs_0_, bf16[256,1024]{1,0:T(8,128)(2,1)S(1)} %collective-permute-done.refs_2_.refs_5_.refs_1_, bf16[256,1024]{1,0:T(8,128)(2,1)S(1)} %get-tuple-element.42.k_ref.refs_2_, ...), custom_call_target="tpu_custom_call" | custom-call | flops 402653184 | bytes 2097152 | tf_op jit(solution)/shard_map/attend_1_1_3/pallas_call | solution.py:435
  47.5 1.6 %collective-permute-start.22 = (bf16[512,512]{1,0:T(8,128)(2,1)S(1)}, bf16[512,512]{1,0:T(8,128)(2,1)S(1)}, u32[]{:S(2)}, u32[]{:S(2)}) collective-permute-start(bf16[512,512]{1,0:T(8,128)(2,1)S(1)} %attend_1_1_3.1.refs_14_.refs_10_), channel_id=1, source_target_pairs={{0,2},{2,0},{1,3},{3,1},{4,6},{6,4},{5,7},{7,5},{8,10},{10,8},{9,1... | collective-permute-start | bytes 1572872 | tf_op jit(solution)/shard_map/ppermute | solution.py:510
  49.0 1.1 %own_carries.1 = (s16[528,128]{1,0:T(8,128)(2,1)S(1)}, s16[528,128]{1,0:T(8,128)(2,1)S(1)}, f32[2,2,128,128]{3,2,1,0:T(8,128)S(1)}, f32[2,2,128,128]{3,2,1,0:T(8,128)S(1)}) custom-call(s32[4]{0:T(128)S(1)} %pad_add_fusion.place_ref, f32[2,128,128]{2,1,0:T(8,128)S(1)} %get-tuple-element.51.refs_0_.own_ref, ...), custom_call_target="tpu_custom_call" | custom-call | bytes 2621440 | tf_op jit(solution)/shard_map/own_carries/pallas_call | solution.py:339
  50.1 0.7 %collective-permute-start.25 = (f32[2,2,128,128]{3,2,1,0:T(8,128)S(1)}, f32[2,2,128,128]{3,2,1,0:T(8,128)S(1)}, u32[]{:S(2)}, u32[]{:S(2)}) collective-permute-start(f32[2,2,128,128]{3,2,1,0:T(8,128)S(1)} %get-tuple-element.69), channel_id=1, source_target_pairs={{0,4},{4,0},{1,5},{5,1},{2,6},{6,2},{3,7},{7,3},{8,12},{12,8},{9,1... | collective-permute-start | bytes 786440 | tf_op jit(solution)/shard_map/ppermute | solution.py:510
  50.9 1.3 %collective-permute-start.23 = (s16[528,128]{1,0:T(8,128)(2,1)S(1)}, s16[528,128]{1,0:T(8,128)(2,1)S(1)}, u32[]{:S(2)}, u32[]{:S(2)}) collective-permute-start(s16[528,128]{1,0:T(8,128)(2,1)S(1)} %get-tuple-element.67), channel_id=1, source_target_pairs={{0,4},{2,6},{4,0},{6,2},{1,5},{3,7},{5,1},{7,3},{8,12},{10,14},{12... | collective-permute-start | bytes 405512 | tf_op jit(solution)/shard_map/ppermute | solution.py:510
  52.2 5.8 %collective-permute-done.23.refs_9_ = s16[528,128]{1,0:T(8,128)(2,1)S(1)} collective-permute-done((s16[528,128]{1,0:T(8,128)(2,1)S(1)}, s16[528,128]{1,0:T(8,128)(2,1)S(1)}, u32[]{:S(2)}, u32[]{:S(2)}) %collective-permute-start.23) | collective-permute-done | bytes 135200 | tf_op jit(solution)/shard_map/ppermute | solution.py:510
  58.0 1.9 %attend_0_0_2.1.refs_10_.refs_0_ = bf16[512,512]{1,0:T(8,128)(2,1)S(1)} custom-call(s32[4]{0:T(128)S(1)} %pad_add_fusion.place_ref, bf16[256,1024]{1,0:T(8,128)(2,1)S(1)} %get-tuple-element.50.refs_1_.q_ref.refs_0_, bf16[256,1024]{1,0:T(8,128)(2,1)S(1)} %collective-permute-done.5.refs_1_.refs_4_.q_sib_ref, ...), custom_call_target="tpu_custom_call" | custom-call | flops 402653184 | bytes 2097152 | tf_op jit(solution)/shard_map/attend_0_0_2/pallas_call | solution.py:435
  59.9 1.9 %attend_1_0_2.1.refs_1_ = bf16[512,512]{1,0:T(8,128)(2,1)S(1)} custom-call(s32[4]{0:T(128)S(1)} %pad_add_fusion.place_ref, bf16[256,1024]{1,0:T(8,128)(2,1)S(1)} %get-tuple-element.40.refs_0_, bf16[256,1024]{1,0:T(8,128)(2,1)S(1)} %collective-permute-done.refs_2_.refs_5_.refs_1_, bf16[256,1024]{1,0:T(8,128)(2,1)S(1)} %get-tuple-element.42.k_ref.refs_2_, ...), custom_call_target="tpu_custom_call" | custom-call | flops 402653184 | bytes 2097152 | tf_op jit(solution)/shard_map/attend_1_0_2/pallas_call | solution.py:435
  61.8 1.4 %assemble_cache.1 = f32[1,8,128,128]{3,2,1,0:T(8,128)} custom-call(s32[4]{0:T(128)S(1)} %pad_add_fusion.place_ref, f32[2,2,128,128]{3,2,1,0:T(8,128)S(1)} %get-tuple-element.68.refs_0_, f32[2,2,128,128]{3,2,1,0:T(8,128)S(1)} %collective-permute-done.25.refs_1_), custom_call_target="tpu_custom_call" | custom-call | tf_op jit(solution)/shard_map/assemble_cache/pallas_call | solution.py:495
  63.2 0.0 collective-permute-done.24.refs_2_
  63.2 1.7 %assemble.1.refs_1_ = bf16[1024,1024]{1,0:T(8,128)(2,1)} custom-call(s32[4]{0:T(128)S(1)} %pad_add_fusion.place_ref, bf16[512,512]{1,0:T(8,128)(2,1)S(1)} %attend_0_0_2.1.refs_10_.refs_0_, bf16[512,512]{1,0:T(8,128)(2,1)S(1)} %attend_1_0_2.1.refs_1_, bf16[512,512]{1,0:T(8,128)(2,1)S(1)} %collective-permute-done.24.refs_2_), custom_call_target="tpu_custom_call" | custom-call | tf_op jit(solution)/shard_map/assemble/pallas_call | solution.py:474
  64.9 1.6 %collective-permute-done.22.refs_0_ = bf16[512,512]{1,0:T(8,128)(2,1)S(1)} collective-permute-done((bf16[512,512]{1,0:T(8,128)(2,1)S(1)}, bf16[512,512]{1,0:T(8,128)(2,1)S(1)}, u32[]{:S(2)}, u32[]{:S(2)}) %collective-permute-start.22) | collective-permute-done | bytes 524320 | tf_op jit(solution)/shard_map/ppermute | solution.py:510
  66.5 1.4 %finish.1 = bf16[1024,1024]{1,0:T(8,128)(2,1)} custom-call(s32[4]{0:T(128)S(1)} %pad_add_fusion.place_ref, bf16[512,512]{1,0:T(8,128)(2,1)S(1)} %collective-permute-done.22.refs_0_, bf16[1024,1024]{1,0:T(8,128)(2,1)} %assemble.1.refs_1_), custom_call_target="tpu_custom_call", output_to_operand_aliasing={{}: (2, {})} | custom-call | tf_op jit(solution)/shard_map/finish/pallas_call | solution.py:474
  (10 shorter events, 0.0 us)
Async XLA Ops:
  0.7 5.0 %copy-start = (bf16[256,4096]{1,0:T(8,128)(2,1)S(1)}, bf16[256,4096]{1,0:T(8,128)(2,1)}, u32[]{:S(2)}) copy-start(bf16[256,4096]{1,0:T(8,128)(2,1)} %queries_ref.1) | copy-start | bytes 6291460
  5.1 2.4 %collective-permute-start.3 = (bf16[256,1024]{1,0:T(8,128)(2,1)S(1)}, bf16[256,1024]{1,0:T(8,128)(2,1)S(1)}, u32[]{:S(2)}, u32[]{:S(2)}) collective-permute-start(bf16[256,1024]{1,0:T(8,128)(2,1)S(1)} %get-tuple-element.47), channel_id=1, source_target_pairs={{0,1},{1,0},{2,3},{3,2},{4,5},{5,4},{6,7},{7,6},{8,9},{9,8},{10,11... | collective-permute-start | bytes 1572872 | tf_op jit(solution)/shard_map/ppermute | solution.py:510
  5.6 2.3 %collective-permute-start.4 = (bf16[256,1024]{1,0:T(8,128)(2,1)S(1)}, bf16[256,1024]{1,0:T(8,128)(2,1)S(1)}, u32[]{:S(2)}, u32[]{:S(2)}) collective-permute-start(bf16[256,1024]{1,0:T(8,128)(2,1)S(1)} %get-tuple-element.49), channel_id=1, source_target_pairs={{0,1},{1,0},{2,3},{3,2},{4,5},{5,4},{6,7},{7,6},{8,9},{9,8},{10,11... | collective-permute-start | bytes 1572872 | tf_op jit(solution)/shard_map/ppermute | solution.py:510
  5.7 2.2 %copy-start.1 = (f32[1024]{0:T(1024)S(1)}, f32[1024]{0:T(1024)}, u32[]{:S(2)}) copy-start(f32[1024]{0:T(1024)} %param.9) | copy-start | bytes 12292
  6.5 5.7 %collective-permute-start = (bf16[256,1024]{1,0:T(8,128)(2,1)S(1)}, bf16[256,1024]{1,0:T(8,128)(2,1)S(1)}, u32[]{:S(2)}, u32[]{:S(2)}) collective-permute-start(bf16[256,1024]{1,0:T(8,128)(2,1)S(1)} %get-tuple-element.41), channel_id=1, source_target_pairs={{0,1},{1,0},{2,3},{3,2},{4,5},{5,4},{6,7},{7,6},{8,9},{9,8},{10,11... | collective-permute-start | bytes 1572872 | tf_op jit(solution)/shard_map/ppermute | solution.py:510
  7.0 6.6 %collective-permute-start.5 = (bf16[256,1024]{1,0:T(8,128)(2,1)S(1)}, bf16[256,1024]{1,0:T(8,128)(2,1)S(1)}, u32[]{:S(2)}, u32[]{:S(2)}) collective-permute-start(bf16[256,1024]{1,0:T(8,128)(2,1)S(1)} %get-tuple-element.52), channel_id=1, source_target_pairs={{0,1},{1,0},{2,3},{3,2},{4,5},{5,4},{6,7},{7,6},{8,9},{9,8},{10,11... | collective-permute-start | bytes 1572872 | tf_op jit(solution)/shard_map/ppermute | solution.py:510
  7.1 6.7 %collective-permute-start.1 = (bf16[256,1024]{1,0:T(8,128)(2,1)S(1)}, bf16[256,1024]{1,0:T(8,128)(2,1)S(1)}, u32[]{:S(2)}, u32[]{:S(2)}) collective-permute-start(bf16[256,1024]{1,0:T(8,128)(2,1)S(1)} %get-tuple-element.43), channel_id=1, source_target_pairs={{0,1},{1,0},{2,3},{3,2},{4,5},{5,4},{6,7},{7,6},{8,9},{9,8},{10,11... | collective-permute-start | bytes 1572872 | tf_op jit(solution)/shard_map/ppermute | solution.py:510
  7.5 6.3 %collective-permute-start.2 = (bf16[256,1024]{1,0:T(8,128)(2,1)S(1)}, bf16[256,1024]{1,0:T(8,128)(2,1)S(1)}, u32[]{:S(2)}, u32[]{:S(2)}) collective-permute-start(bf16[256,1024]{1,0:T(8,128)(2,1)S(1)} %get-tuple-element.45), channel_id=1, source_target_pairs={{0,1},{1,0},{2,3},{3,2},{4,5},{5,4},{6,7},{7,6},{8,9},{9,8},{10,11... | collective-permute-start | bytes 1572872 | tf_op jit(solution)/shard_map/ppermute | solution.py:510
  9.3 10.0 %collective-permute-start.6 = (s16[288,128]{1,0:T(8,128)(2,1)S(1)}, s16[288,128]{1,0:T(8,128)(2,1)S(1)}, u32[]{:S(2)}, u32[]{:S(2)}) collective-permute-start(s16[288,128]{1,0:T(8,128)(2,1)S(1)} %get-tuple-element.54), channel_id=1, source_target_pairs={{0,2},{2,0},{4,6},{6,4},{1,3},{3,1},{5,7},{7,5},{8,10},{10,8},{12,... | collective-permute-start | bytes 221192 | tf_op jit(solution)/shard_map/ppermute | solution.py:510
  12.2 6.4 %collective-permute-start.10 = (s16[272,128]{1,0:T(8,128)(2,1)S(1)}, s16[272,128]{1,0:T(8,128)(2,1)S(1)}, u32[]{:S(2)}, u32[]{:S(2)}) collective-permute-start(s16[272,128]{1,0:T(8,128)(2,1)S(1)} %get-tuple-element.59), channel_id=1, source_target_pairs={{0,6},{2,4},{4,2},{6,0},{1,7},{3,5},{5,3},{7,1},{8,14},{10,12},{12... | collective-permute-start | bytes 208904 | tf_op jit(solution)/shard_map/ppermute | solution.py:510
  13.7 5.6 %collective-permute-start.11 = (s16[272,128]{1,0:T(8,128)(2,1)S(1)}, s16[272,128]{1,0:T(8,128)(2,1)S(1)}, u32[]{:S(2)}, u32[]{:S(2)}) collective-permute-start(s16[272,128]{1,0:T(8,128)(2,1)S(1)} %get-tuple-element.60), channel_id=1, source_target_pairs={{0,4},{2,6},{4,0},{6,2},{1,5},{3,7},{5,1},{7,3},{8,12},{10,14},{12... | collective-permute-start | bytes 208904 | tf_op jit(solution)/shard_map/ppermute | solution.py:510
  15.2 11.0 %collective-permute-start.7 = (s16[272,128]{1,0:T(8,128)(2,1)S(1)}, s16[272,128]{1,0:T(8,128)(2,1)S(1)}, u32[]{:S(2)}, u32[]{:S(2)}) collective-permute-start(s16[272,128]{1,0:T(8,128)(2,1)S(1)} %get-tuple-element.56), channel_id=1, source_target_pairs={{0,2},{2,0},{4,6},{6,4},{1,3},{3,1},{5,7},{7,5},{8,10},{10,8},{12,... | collective-permute-start | bytes 208904 | tf_op jit(solution)/shard_map/ppermute | solution.py:510
  17.2 11.5 %collective-permute-start.8 = (s16[272,128]{1,0:T(8,128)(2,1)S(1)}, s16[272,128]{1,0:T(8,128)(2,1)S(1)}, u32[]{:S(2)}, u32[]{:S(2)}) collective-permute-start(s16[272,128]{1,0:T(8,128)(2,1)S(1)} %get-tuple-element.57), channel_id=1, source_target_pairs={{0,4},{2,6},{4,0},{6,2},{1,5},{3,7},{5,1},{7,3},{8,12},{10,14},{12... | collective-permute-start | bytes 208904 | tf_op jit(solution)/shard_map/ppermute | solution.py:510
  18.7 10.0 %collective-permute-start.9 = (s16[272,128]{1,0:T(8,128)(2,1)S(1)}, s16[272,128]{1,0:T(8,128)(2,1)S(1)}, u32[]{:S(2)}, u32[]{:S(2)}) collective-permute-start(s16[272,128]{1,0:T(8,128)(2,1)S(1)} %get-tuple-element.58), channel_id=1, source_target_pairs={{0,6},{2,4},{4,2},{6,0},{1,7},{3,5},{5,3},{7,1},{8,14},{10,12},{12... | collective-permute-start | bytes 208904 | tf_op jit(solution)/shard_map/ppermute | solution.py:510
  19.4 12.0 %collective-permute-start.17 = (s16[272,128]{1,0:T(8,128)(2,1)S(1)}, s16[272,128]{1,0:T(8,128)(2,1)S(1)}, u32[]{:S(2)}, u32[]{:S(2)}) collective-permute-start(s16[272,128]{1,0:T(8,128)(2,1)S(1)} %level_states_0.1.refs_3_), channel_id=1, source_target_pairs={{0,24},{1,25},{2,26},{3,27},{4,28},{5,29},{6,30},{7,31}} | collective-permute-start | bytes 208904 | tf_op jit(solution)/shard_map/ppermute | solution.py:517
  24.9 9.9 %collective-permute-start.16 = (s16[272,128]{1,0:T(8,128)(2,1)S(1)}, s16[272,128]{1,0:T(8,128)(2,1)S(1)}, u32[]{:S(2)}, u32[]{:S(2)}) collective-permute-start(s16[272,128]{1,0:T(8,128)(2,1)S(1)} %level_states_0.1.refs_3_), channel_id=1, source_target_pairs={{0,16},{8,24},{1,17},{9,25},{2,18},{10,26},{3,19},{11,27},{4,20},{... | collective-permute-start | bytes 208904 | tf_op jit(solution)/shard_map/ppermute | solution.py:517
  26.2 8.6 %collective-permute-start.15 = (s16[272,128]{1,0:T(8,128)(2,1)S(1)}, s16[272,128]{1,0:T(8,128)(2,1)S(1)}, u32[]{:S(2)}, u32[]{:S(2)}) collective-permute-start(s16[272,128]{1,0:T(8,128)(2,1)S(1)} %level_states_0.1.refs_3_), channel_id=1, source_target_pairs={{0,8},{8,16},{16,24},{1,9},{9,17},{17,25},{2,10},{10,18},{18,26},{... | collective-permute-start | bytes 208904 | tf_op jit(solution)/shard_map/ppermute | solution.py:517
  28.8 9.1 %collective-permute-start.14 = (s16[272,128]{1,0:T(8,128)(2,1)S(1)}, s16[272,128]{1,0:T(8,128)(2,1)S(1)}, u32[]{:S(2)}, u32[]{:S(2)}) collective-permute-start(s16[272,128]{1,0:T(8,128)(2,1)S(1)} %level_states_1.1.refs_0_), channel_id=1, source_target_pairs={{0,24},{1,25},{2,26},{3,27},{4,28},{5,29},{6,30},{7,31}} | collective-permute-start | bytes 208904 | tf_op jit(solution)/shard_map/ppermute | solution.py:517
  30.1 7.8 %collective-permute-start.13 = (s16[272,128]{1,0:T(8,128)(2,1)S(1)}, s16[272,128]{1,0:T(8,128)(2,1)S(1)}, u32[]{:S(2)}, u32[]{:S(2)}) collective-permute-start(s16[272,128]{1,0:T(8,128)(2,1)S(1)} %level_states_1.1.refs_0_), channel_id=1, source_target_pairs={{0,16},{8,24},{1,17},{9,25},{2,18},{10,26},{3,19},{11,27},{4,20},{... | collective-permute-start | bytes 208904 | tf_op jit(solution)/shard_map/ppermute | solution.py:517
  31.4 6.5 %collective-permute-start.12 = (s16[272,128]{1,0:T(8,128)(2,1)S(1)}, s16[272,128]{1,0:T(8,128)(2,1)S(1)}, u32[]{:S(2)}, u32[]{:S(2)}) collective-permute-start(s16[272,128]{1,0:T(8,128)(2,1)S(1)} %level_states_1.1.refs_0_), channel_id=1, source_target_pairs={{0,8},{8,16},{16,24},{1,9},{9,17},{17,25},{2,10},{10,18},{18,26},{... | collective-permute-start | bytes 208904 | tf_op jit(solution)/shard_map/ppermute | solution.py:517
  35.5 5.9 %collective-permute-start.21 = (s16[272,128]{1,0:T(8,128)(2,1)S(1)}, s16[272,128]{1,0:T(8,128)(2,1)S(1)}, u32[]{:S(2)}, u32[]{:S(2)}) collective-permute-start(s16[272,128]{1,0:T(8,128)(2,1)S(1)} %get-tuple-element.65), channel_id=1, source_target_pairs={{0,6},{2,4},{4,2},{6,0},{1,7},{3,5},{5,3},{7,1},{8,14},{10,12},{12... | collective-permute-start | bytes 208904 | tf_op jit(solution)/shard_map/ppermute | solution.py:510
  37.4 5.2 %collective-permute-start.20 = (s16[272,128]{1,0:T(8,128)(2,1)S(1)}, s16[272,128]{1,0:T(8,128)(2,1)S(1)}, u32[]{:S(2)}, u32[]{:S(2)}) collective-permute-start(s16[272,128]{1,0:T(8,128)(2,1)S(1)} %get-tuple-element.61.refs_6_), channel_id=1, source_target_pairs={{0,2},{2,0},{4,6},{6,4},{1,3},{3,1},{5,7},{7,5},{8,10},{10,8},{12,... | collective-permute-start | bytes 208904 | tf_op jit(solution)/shard_map/ppermute | solution.py:510
  38.7 6.7 %collective-permute-start.19 = (s16[272,128]{1,0:T(8,128)(2,1)S(1)}, s16[272,128]{1,0:T(8,128)(2,1)S(1)}, u32[]{:S(2)}, u32[]{:S(2)}) collective-permute-start(s16[272,128]{1,0:T(8,128)(2,1)S(1)} %get-tuple-element.63), channel_id=1, source_target_pairs={{0,6},{2,4},{4,2},{6,0},{1,7},{3,5},{5,3},{7,1},{8,14},{10,12},{12... | collective-permute-start | bytes 208904 | tf_op jit(solution)/shard_map/ppermute | solution.py:510
  40.3 5.2 %collective-permute-start.18 = (s16[272,128]{1,0:T(8,128)(2,1)S(1)}, s16[272,128]{1,0:T(8,128)(2,1)S(1)}, u32[]{:S(2)}, u32[]{:S(2)}) collective-permute-start(s16[272,128]{1,0:T(8,128)(2,1)S(1)} %get-tuple-element.62.refs_7_), channel_id=1, source_target_pairs={{0,2},{2,0},{4,6},{6,4},{1,3},{3,1},{5,7},{7,5},{8,10},{10,8},{12,... | collective-permute-start | bytes 208904 | tf_op jit(solution)/shard_map/ppermute | solution.py:510
  43.8 19.4 %collective-permute-start.24 = (bf16[512,512]{1,0:T(8,128)(2,1)S(1)}, bf16[512,512]{1,0:T(8,128)(2,1)S(1)}, u32[]{:S(2)}, u32[]{:S(2)}) collective-permute-start(bf16[512,512]{1,0:T(8,128)(2,1)S(1)} %attend_0_1_3.1.refs_10_), channel_id=1, source_target_pairs={{0,2},{2,0},{1,3},{3,1},{4,6},{6,4},{5,7},{7,5},{8,10},{10,8},{9,1... | collective-permute-start | bytes 1572872 | tf_op jit(solution)/shard_map/ppermute | solution.py:510
  47.5 19.0 %collective-permute-start.22 = (bf16[512,512]{1,0:T(8,128)(2,1)S(1)}, bf16[512,512]{1,0:T(8,128)(2,1)S(1)}, u32[]{:S(2)}, u32[]{:S(2)}) collective-permute-start(bf16[512,512]{1,0:T(8,128)(2,1)S(1)} %attend_1_1_3.1.refs_14_.refs_10_), channel_id=1, source_target_pairs={{0,2},{2,0},{1,3},{3,1},{4,6},{6,4},{5,7},{7,5},{8,10},{10,8},{9,1... | collective-permute-start | bytes 1572872 | tf_op jit(solution)/shard_map/ppermute | solution.py:510
  50.1 11.6 %collective-permute-start.25 = (f32[2,2,128,128]{3,2,1,0:T(8,128)S(1)}, f32[2,2,128,128]{3,2,1,0:T(8,128)S(1)}, u32[]{:S(2)}, u32[]{:S(2)}) collective-permute-start(f32[2,2,128,128]{3,2,1,0:T(8,128)S(1)} %get-tuple-element.69), channel_id=1, source_target_pairs={{0,4},{4,0},{1,5},{5,1},{2,6},{6,2},{3,7},{7,3},{8,12},{12,8},{9,1... | collective-permute-start | bytes 786440 | tf_op jit(solution)/shard_map/ppermute | solution.py:510
  50.9 7.1 %collective-permute-start.23 = (s16[528,128]{1,0:T(8,128)(2,1)S(1)}, s16[528,128]{1,0:T(8,128)(2,1)S(1)}, u32[]{:S(2)}, u32[]{:S(2)}) collective-permute-start(s16[528,128]{1,0:T(8,128)(2,1)S(1)} %get-tuple-element.67), channel_id=1, source_target_pairs={{0,4},{2,6},{4,0},{6,2},{1,5},{3,7},{5,1},{7,3},{8,12},{10,14},{12... | collective-permute-start | bytes 405512 | tf_op jit(solution)/shard_map/ppermute | solution.py:510

commit v15 on v14

--- a/solution.py
+++ b/solution.py
@@ -17,7 +17,6 @@
 TOP = 32767.0
 
 VMEM = pl.BlockSpec(memory_space=pltpu.VMEM)
-SMEM = pl.BlockSpec(memory_space=pltpu.SMEM)
 HBM = pl.BlockSpec(memory_space=pltpu.HBM)
 ANY = pl.BlockSpec(memory_space=pl.ANY)
 
@@ -28,6 +27,14 @@
 
 def cost(flops, bytes_accessed):
     return pl.CostEstimate(flops=flops, bytes_accessed=bytes_accessed, transcendentals=0)
+
+
+def at_place(kernel):
+    def placed(*refs):
+        place = [lax.axis_index(a) for a in ("core", "inner", "y", "outer")]
+        kernel(place, *refs)
+
+    return placed
 
 
 class Plan:
@@ -60,24 +67,25 @@
     return value, key, rest - 3 * key
 
 
-def sides(plan, place_ref):
+def sides(plan, core):
     width = plan.half_width
     for y in range(plan.n_y):
         for side in range(CORES):
-            of = place_ref[0] if side == 0 else 1 - place_ref[0]
+            of = core if side == 0 else 1 - core
             for half in range(plan.halves):
                 start = ((y * CORES + of) * plan.halves + half) * width
                 at = pl.ds(pl.multiple_of(start, width), width)
                 yield side, half, slice(y * width, (y + 1) * width), at
 
 
-def decode(plan, place, spikes, keys, values):
+def decode(plan, spikes, keys, values):
     rows, model = spikes.shape
     step = min(rows, 32)
     chunks = rows // step
     n_out = 3 * CORES * plan.halves
 
-    def kernel(place_ref, *refs):
+    def kernel(*refs):
+        core = lax.axis_index("core")
         sources, *outs, b0, b1, b2, sems = refs[:3], *refs[3:]
         buffers = (b0, b1, b2)
 
@@ -96,7 +104,7 @@
             for index in range(3):
                 fetch(chunk, index).wait()
             at = pl.ds(pl.multiple_of(chunk * step, step), step)
-            for side, half, mine, columns in sides(plan, place_ref):
+            for side, half, mine, columns in sides(plan, core):
                 spikes = buffers[0][at, columns].astype(jnp.float32).astype(jnp.bfloat16)
                 value, key, query = counts_of(spikes)
                 spiked = (buffers[1][at, columns] * key, buffers[2][at, columns] * value, query)
@@ -106,7 +114,7 @@
     return pl.pallas_call(
         kernel,
         out_shape=[jax.ShapeDtypeStruct((rows, plan.n_y * plan.half_width), jnp.bfloat16)] * n_out,
-        in_specs=[SMEM] + [HBM] * 3,
+        in_specs=[HBM] * 3,
         out_specs=[VMEM] * n_out,
         scratch_shapes=[
             pltpu.VMEM((rows, model), jnp.int32),
@@ -117,26 +125,26 @@
         compiler_params=params(DECODE_VMEM_BYTES),
         cost_estimate=cost(rows * model * 4, rows * model * 14),
         name="decode",
-    )(place, spikes, keys, values)
-
-
-def spike_queries(plan, place, queries, counts):
+    )(spikes, keys, values)
+
+
+def spike_queries(plan, queries, counts):
     n = len(counts)
 
     def kernel(place_ref, queries_ref, *refs):
-        for side, half, mine, columns in sides(plan, place_ref):
+        for side, half, mine, columns in sides(plan, place_ref[0]):
             at = side * plan.halves + half
             refs[n + at][:, mine] = queries_ref[:, columns] * refs[at][:, mine]
 
     return pl.pallas_call(
-        kernel,
+        at_place(kernel),
         out_shape=[jax.ShapeDtypeStruct(a.shape, jnp.bfloat16) for a in counts],
-        in_specs=[SMEM] + [VMEM] * (1 + n),
+        in_specs=[VMEM] * (1 + n),
         out_specs=[VMEM] * n,
         compiler_params=params(),
         cost_estimate=cost(queries.size, queries.size * 6),
         name="spike_queries",
-    )(place, queries, *counts)
+    )(queries, *counts)
 
 
 def contract_rows(left, right):
@@ -217,7 +225,7 @@
     return pl.ds(pl.multiple_of(start, HD), HD)
 
 
-def chunk_states(plan, place, key, value, half, after, gain=None):
+def chunk_states(plan, key, value, half, after, gain=None):
     gains = [] if gain is None else [gain]
 
     def kernel(place_ref, k_ref, k_sib_ref, v_ref, v_sib_ref, *refs):
@@ -241,20 +249,20 @@
 
     heads = plan.plane * plan.each
     return pl.pallas_call(
-        kernel,
+        at_place(kernel),
         out_shape=[states_shape(plan.each), states_shape(plan.plane, plan.each)]
         + [
             coded_shape(plan.each, PAD if gains and o < plan.n_y else 0)
             for o in range(1, plan.plane)
         ],
-        in_specs=[SMEM] + [VMEM] * (4 + len(gains)) + [ANY] * len(after),
+        in_specs=[VMEM] * (4 + len(gains)) + [ANY] * len(after),
         out_specs=[VMEM] * (1 + plan.plane),
         compiler_params=params(),
         cost_estimate=cost(
             4 * plan.rows * HD * HD * heads, 8 * plan.rows * HD * heads + 6 * heads * HD * HD
         ),
         name=f"chunk_states_{half}",
-    )(place, *key, *value, *gains, *after)
+    )(*key, *value, *gains, *after)
 
 
 def level_states(plan, own, others, half, after):
@@ -292,7 +300,7 @@
     return before, blocks
 
 
-def carries(plan, place, own, others, levels, half, offsets, after):
+def carries(plan, own, others, levels, half, offsets, after):
     n_others, n_levels = len(others), len(levels)
 
     def kernel(place_ref, own_ref, *refs):
@@ -303,17 +311,17 @@
             code(states, ref)
 
     return pl.pallas_call(
-        kernel,
+        at_place(kernel),
         out_shape=[coded_shape(plan.each)] * len(offsets),
-        in_specs=[SMEM] + [VMEM] * (1 + n_others + n_levels) + [ANY] * len(after),
+        in_specs=[VMEM] * (1 + n_others + n_levels) + [ANY] * len(after),
         out_specs=[VMEM] * len(offsets),
         compiler_params=params(),
         cost_estimate=cost(0, (plan.plane * 4 + n_levels) * plan.each * HD * HD * 2),
         name=f"carries_{half}",
-    )(place, own, *others, *levels, *after)
-
-
-def own_carries(plan, place, own, others, levels, offsets, after):
+    )(own, *others, *levels, *after)
+
+
+def own_carries(plan, own, others, levels, offsets, after):
     n_others = len(others[0])
     operands = [(own[h], *others[h], *levels[h]) for h in range(plan.halves)]
     starts = [sum(map(len, operands[:h])) for h in range(plan.halves + 1)]
@@ -337,38 +345,15 @@
             code(states, ref)
 
     return pl.pallas_call(
-        kernel,
+        at_place(kernel),
         out_shape=[coded_shape(plan.halves * plan.each)] * len(offsets)
         + [states_shape(plan.halves, plan.each)] * plan.n_inner,
-        in_specs=[SMEM] + [VMEM] * starts[-1] + [ANY] * len(after),
+        in_specs=[VMEM] * starts[-1] + [ANY] * len(after),
         out_specs=[VMEM] * (len(offsets) + plan.n_inner),
         compiler_params=params(),
         cost_estimate=cost(0, plan.plane * plan.each * HD * HD * 20),
         name="own_carries",
-    )(place, *[a for arrays in operands for a in arrays], *after)
-
-
-def attend_local(plan, place, query, key, value, half, offsets, after):
-    rows = plan.rows
-
-    def kernel(place_ref, q_ref, q_sib_ref, k_ref, k_sib_ref, v_ref, v_sib_ref, *refs):
-        for piece, offset in enumerate(offsets):
-            for i in range(plan.each):
-                at = owned_columns(plan, place_ref, offset, i)
-                out_at = slice(piece * plan.piece + i * HD, piece * plan.piece + (i + 1) * HD)
-                refs[-1][0, :, out_at] = local_part(q_ref, k_ref, v_ref, at)
-                refs[-1][1, :, out_at] = local_part(q_sib_ref, k_sib_ref, v_sib_ref, at)
-
-    heads = len(offsets) * plan.each
-    return pl.pallas_call(
-        kernel,
-        out_shape=jax.ShapeDtypeStruct((CORES, rows, heads * HD), jnp.float32),
-        in_specs=[SMEM] + [VMEM] * 6 + [ANY] * len(after),
-        out_specs=VMEM,
-        compiler_params=params(),
-        cost_estimate=cost(heads * 8 * rows * rows * HD, 16 * rows * heads * HD),
-        name=f"attend_local_{half}_" + "_".join(map(str, offsets)),
-    )(place, *query, *key, *value, *after)
+    )(*[a for arrays in operands for a in arrays], *after)
 
 
 def local_part(q_ref, k_ref, v_ref, at):
@@ -391,11 +376,9 @@
     return (raw * lax.rsqrt(mean + 1e-06) * gain).astype(jnp.bfloat16)
 
 
-def attend(
-    plan, place, query, key, value, carry, first, gain, half, offsets, after=(), local=None
-):
+def attend(plan, query, key, value, carry, first, gain, half, offsets, after):
     rows = plan.rows
-    operands = [*query, local] if local is not None else [*query, *key, *value]
+    operands = [*query, *key, *value]
     n = len(operands)
 
     def kernel(place_ref, *refs):
@@ -421,10 +404,7 @@
                 carried = carry_states[skip + i]
                 first = first_ref[offset, i]
                 for side in range(CORES):
-                    if local is None:
-                        raw = local_part(refs[side], refs[2 + side], refs[4 + side], at)
-                    else:
-                        raw = refs[2][side, :, out_at]
+                    raw = local_part(refs[side], refs[2 + side], refs[4 + side], at)
                     behind = is_second if side == 0 else ~is_second
                     state = carried + jnp.where(behind, first, 0.0)
                     of = core if side == 0 else 1 - core
@@ -433,19 +413,19 @@
 
     heads = len(offsets) * plan.each
     return pl.pallas_call(
-        kernel,
+        at_place(kernel),
         out_shape=jax.ShapeDtypeStruct((CORES * rows, heads * HD), jnp.bfloat16),
-        in_specs=[SMEM] + [VMEM] * (n + 2 + len(offsets)) + [ANY] * len(after),
+        in_specs=[VMEM] * (n + 2 + len(offsets)) + [ANY] * len(after),
         out_specs=VMEM,
         compiler_params=params(),
         cost_estimate=cost(
             heads * (8 * rows * rows * HD + 8 * rows * HD * HD), 16 * rows * heads * HD
         ),
         name=f"attend_{half}_" + "_".join(map(str, offsets)),
-    )(place, *operands, first, gain, *carry, *after)
-
-
-def assemble(plan, place, parts, into=None):
+    )(*operands, first, gain, *carry, *after)
+
+
+def assemble(plan, parts, into=None):
     rows = CORES * plan.rows
     copies = [(n, piece, half, o) for n, (_, half, os) in enumerate(parts) for piece, o in enumerate(os)]
 
@@ -472,18 +452,18 @@
     arrays = [array for array, _, _ in parts]
     aliased = [] if into is None else [into]
     return pl.pallas_call(
-        kernel,
+        at_place(kernel),
         out_shape=jax.ShapeDtypeStruct((plan.n_y * rows, plan.width), jnp.bfloat16),
-        in_specs=[SMEM] + [VMEM] * len(arrays) + [HBM] * len(aliased),
+        in_specs=[VMEM] * len(arrays) + [HBM] * len(aliased),
         out_specs=HBM,
         scratch_shapes=[pltpu.SemaphoreType.DMA((len(copies),))],
-        input_output_aliases={1 + len(arrays): 0} if aliased else {},
+        input_output_aliases={len(arrays): 0} if aliased else {},
         compiler_params=params(),
         name="assemble" if into is None else "finish",
-    )(place, *arrays, *aliased)
-
-
-def assemble_cache(plan, place, parts):
+    )(*arrays, *aliased)
+
+
+def assemble_cache(plan, parts):
     group = plan.n_inner * plan.each
 
     def kernel(place_ref, *refs):
@@ -493,17 +473,16 @@
                 refs[-1][0, pl.ds(start, plan.each)] = ref[half]
 
     return pl.pallas_call(
-        kernel,
+        at_place(kernel),
         out_shape=states_shape(1, plan.halves * group),
-        in_specs=[SMEM] + [VMEM] * len(parts),
+        in_specs=[VMEM] * len(parts),
         out_specs=VMEM,
         compiler_params=params(),
         name="assemble_cache",
-    )(place, *parts)
+    )(*parts)
 
 
 def per_device(plan, queries, keys, values, spikes, gain):
-    place = jnp.stack([lax.axis_index(a) for a in ("core", "inner", "y", "outer")]).astype(jnp.int32)
     halves = range(plan.halves)
 
     def swap(array, axes, offset, size):
@@ -517,14 +496,14 @@
         return lax.ppermute(array, "outer", pairs)
 
     gain = gain.reshape(1, plan.width)
-    arrays = decode(plan, place, spikes, keys, values)
+    arrays = decode(plan, spikes, keys, values)
     parts = [arrays[k : k + plan.halves] for k in range(0, len(arrays), plan.halves)]
 
     def with_siblings(mine, theirs):
         return [(a, swap(b, "core", 1, CORES)) for a, b in zip(mine, theirs)]
 
     key, value = with_siblings(*parts[0:2]), with_siblings(*parts[2:4])
-    spiked = spike_queries(plan, place, queries, [*parts[4], *parts[5]])
+    spiked = spike_queries(plan, queries, [*parts[4], *parts[5]])
     query = with_siblings(spiked[: plan.halves], spiked[plan.halves :])
 
     own, first, others = [], [], []
@@ -532,7 +511,7 @@
     def owner_stage(half, after):
         with_gain = gain if half == 0 else None
         mine, of_first, *sends = chunk_states(
-            plan, place, key[half], value[half], half, after, with_gain
+            plan, key[half], value[half], half, after, with_gain
         )
         own.append(mine)
         first.append(of_first)
@@ -541,10 +520,9 @@
     of_group = [list(range(y, plan.plane, plan.n_y)) for y in range(plan.n_y)]
     abroad = [o for offsets in of_group[1:] for o in offsets]
 
-    def part_of(half, offsets, carry, after, local=None):
+    def part_of(half, offsets, carry, after):
         return attend(
             plan,
-            place,
             query[half],
             key[half],
             value[half],
@@ -554,18 +532,17 @@
             half,
             offsets,
             after,
-            local,
         )
 
     def carry_stage(half, after):
-        sends = carries(plan, place, own[half], others[half], levels[half], half, abroad, after)
+        sends = carries(plan, own[half], others[half], levels[half], half, abroad, after)
         return sends[0], {o: in_level(a, o) for o, a in zip(abroad, sends)}
 
     parts = []
 
-    def send_stage(half, carry, after, local):
+    def send_stage(half, carry, after):
         for y in range(1, plan.n_y):
-            part = part_of(half, of_group[y], carry, after, local.get(y))
+            part = part_of(half, of_group[y], carry, after)
             parts.append((swap(part, "y", y, plan.n_y), half, of_group[y]))
             after = [part]
         return after
@@ -579,18 +556,14 @@
         level = level_states(plan, own[half], others[half][::-1], half, after)
         levels.append([to_later(level, d) for d in range(1, plan.n_outer)])
         after = [level]
-    local = {}
-    for y in range(1, plan.n_y):
-        local[y] = attend_local(plan, place, query[0], key[0], value[0], 0, of_group[y], after)
-        after = [local[y]]
     carry = []
     for half in halves:
         done, of_half = carry_stage(half, after)
         carry.append(of_half)
         after = [done]
     for half in halves:
-        after = send_stage(half, carry[half], after, {} if half else local)
-    sends = own_carries(plan, place, own, others, levels, of_group[0], after)
+        after = send_stage(half, carry[half], after)
+    sends = own_carries(plan, own, others, levels, of_group[0], after)
     own_carry = {o: in_level(a, o) if o else a for o, a in zip(of_group[0], sends)}
     caches = [
         swap(a, "inner", o, plan.n_inner) if o else a
@@ -601,9 +574,9 @@
         part = part_of(half, of_group[0], own_carry, after)
         early.append((part, half, of_group[0]))
         after = [part]
-    out = assemble(plan, place, early + parts[:-1])
-    out = assemble(plan, place, parts[-1:], out)
-    return out, assemble_cache(plan, place, caches)
+    out = assemble(plan, early + parts[:-1])
+    out = assemble(plan, parts[-1:], out)
+    return out, assemble_cache(plan, caches)
 
 
 def solution(mesh):

time: 68.1 us -> 63.6 us (0.934)
  Pallas kernels: 23.4 us -> 15.1 us
  waiting for transfers between devices: 9.22 us -> 13.5 us
    pallas_call x14 -> x13, Pallas kernels: 18.9 us -> 11 us  [the longest x4 5.3 us: attend(): pl.pallas_call(at_place(kernel), out_shape=jax.ShapeDtypeStruct((CORES *...]
    ppermute x20, waiting for transfers between devices: 9.2 us -> 13.5 us  [swap(): return lax.ppermute(array, axes, [(i, i ^ offset) for i in range(size)])]
  transfers between devices with their start and end apart: 26 -> 26, of which waited for: 5 -> 6; matrix products, arithmetic and copies ran while one was open for 0% -> 0% of each run, Pallas kernels for 26% -> 17%
where the time goes in v15:
time: 63.6 us; the launch traced here: 63.2 us
  starting transfers between devices  33.7 us (53%)
  Pallas kernels  15.1 us (24%)
  waiting for transfers between devices  13.5 us (21%)
  between operations  0.85 us (1%)
    ppermute x20, starting transfers between devices, swap(): return lax.ppermute(array, axes, [(i, i ^ offset) for i in range(size)])  20.5 us
    ppermute x20, waiting for transfers between devices, swap(): return lax.ppermute(array, axes, [(i, i ^ offset) for i in range(size)])  13.5 us
    ppermute x6, starting transfers between devices, to_later(): return lax.ppermute(array, 'outer', pairs)  13.2 us
    pallas_call x4, Pallas kernels, attend(): pl.pallas_call(at_place(kernel), out_shape=jax.ShapeDtypeStruct((CORES *...  5.3 us
    pallas_call x1, Pallas kernels, decode(): pl.pallas_call(kernel, out_shape=[jax.ShapeDtypeStruct((rows, plan.n_y *...  3.88 us
    pallas_call x2, Pallas kernels, assemble(): pl.pallas_call(at_place(kernel), out_shape=jax.ShapeDtypeStruct((plan.n_y...  1.99 us
    pallas_call x2, Pallas kernels, chunk_states(): pl.pallas_call(at_place(kernel), out_shape=[states_shape(plan.each), stat...  1.64 us
  transfers between devices with their start and end apart: 26, of which 6 were waited for; matrix products, arithmetic and copies ran while one was open for 0% of the time, Pallas kernels for 17%

profile of v15, /device:TPU:0, one launch (start us, length us, event | category | flops | bytes accessed | tf_op | source)
XLA Modules:
  0.0 63.2 jit_solution(17942985074120432768)
XLA Ops:
  0.6 3.9 %decode.1 = (bf16[256,1024]{1,0:T(8,128)(2,1)S(1)}, bf16[256,1024]{1,0:T(8,128)(2,1)S(1)}, bf16[256,1024]{1,0:T(8,128)(2,1)S(1)}, bf16[256,1024]{1,0:T(8,128)(2,...) custom-call(s32[256,4096]{1,0:T(8,128)} %refs_0_.2, ...), custom_call_target="tpu_custom_call" | custom-call | flops 4194304 | bytes 14680064 | tf_op jit(solution)/shard_map/decode/pallas_call | solution.py:114
  4.5 0.5 collective-permute-start.3
  5.1 0.1 collective-permute-start.4
  5.1 0.3 spike_queries.1
  5.4 0.5 collective-permute-start
  5.9 0.1 collective-permute-start.5
  6.0 0.4 collective-permute-start.1
  6.4 0.2 collective-permute-done.3.refs_1_.refs_3_
  6.6 0.4 collective-permute-start.2
  7.0 0.4 collective-permute-done.4.refs_3_.refs_5_
  7.3 0.8 %chunk_states_0.1 = (f32[2,128,128]{2,1,0:T(8,128)S(1)}, f32[4,2,128,128]{3,2,1,0:T(8,128)S(1)}, s16[288,128]{1,0:T(8,128)(2,1)S(1)}, s16[272,128]{1,0:T(8,128)(2,1)S(1)}, s16[272,128]{1,0:T(8,128)(2,1)S(1)}) custom-call(bf16[256,1024]{1,0:T(8,128)(2,1)S(1)} %get-tuple-element.46.refs_0_.refs_2_, ...), custom_call_target="tpu_custom_call" | custom-call | flops 134217728 | bytes 2883584 | tf_op jit(solution)/shard_map/chunk_states_0/pallas_call | solution.py:251
  8.2 3.0 %collective-permute-start.6 = (s16[288,128]{1,0:T(8,128)(2,1)S(1)}, s16[288,128]{1,0:T(8,128)(2,1)S(1)}, u32[]{:S(2)}, u32[]{:S(2)}) collective-permute-start(s16[288,128]{1,0:T(8,128)(2,1)S(1)} %get-tuple-element.54), channel_id=1, source_target_pairs={{0,2},{2,0},{4,6},{6,4},{1,3},{3,1},{5,7},{7,5},{8,10},{10,8},{12,... | collective-permute-start | bytes 221192 | tf_op jit(solution)/shard_map/ppermute | solution.py:489
  11.1 0.0 collective-permute-done.refs_6_.refs_5_.refs_1_
  11.1 1.4 %collective-permute-start.10 = (s16[272,128]{1,0:T(8,128)(2,1)S(1)}, s16[272,128]{1,0:T(8,128)(2,1)S(1)}, u32[]{:S(2)}, u32[]{:S(2)}) collective-permute-start(s16[272,128]{1,0:T(8,128)(2,1)S(1)} %get-tuple-element.59), channel_id=1, source_target_pairs={{0,6},{2,4},{4,2},{6,0},{1,7},{3,5},{5,3},{7,1},{8,14},{10,12},{12... | collective-permute-start | bytes 208904 | tf_op jit(solution)/shard_map/ppermute | solution.py:489
  12.6 0.0 collective-permute-done.5.refs_5_.refs_4_.refs_1_
  12.6 0.1 collective-permute-start.11
  12.7 0.0 collective-permute-done.1.refs_1_.refs_3_
  12.7 0.8 %chunk_states_1.1 = (f32[2,128,128]{2,1,0:T(8,128)S(1)}, f32[4,2,128,128]{3,2,1,0:T(8,128)S(1)}, s16[272,128]{1,0:T(8,128)(2,1)S(1)}, s16[272,128]{1,0:T(8,128)(2,1)S(1)}, s16[272,128]{1,0:T(8,128)(2,1)S(1)}) custom-call(bf16[256,1024]{1,0:T(8,128)(2,1)S(1)} %get-tuple-element.42.refs_0_.refs_2_, ...), custom_call_target="tpu_custom_call" | custom-call | flops 134217728 | bytes 2883584 | tf_op jit(solution)/shard_map/chunk_states_1/pallas_call | solution.py:251
  13.5 2.0 %collective-permute-start.7 = (s16[272,128]{1,0:T(8,128)(2,1)S(1)}, s16[272,128]{1,0:T(8,128)(2,1)S(1)}, u32[]{:S(2)}, u32[]{:S(2)}) collective-permute-start(s16[272,128]{1,0:T(8,128)(2,1)S(1)} %get-tuple-element.56), channel_id=1, source_target_pairs={{0,2},{2,0},{4,6},{6,4},{1,3},{3,1},{5,7},{7,5},{8,10},{10,8},{12,... | collective-permute-start | bytes 208904 | tf_op jit(solution)/shard_map/ppermute | solution.py:489
  15.5 1.5 %collective-permute-start.8 = (s16[272,128]{1,0:T(8,128)(2,1)S(1)}, s16[272,128]{1,0:T(8,128)(2,1)S(1)}, u32[]{:S(2)}, u32[]{:S(2)}) collective-permute-start(s16[272,128]{1,0:T(8,128)(2,1)S(1)} %get-tuple-element.57), channel_id=1, source_target_pairs={{0,4},{2,6},{4,0},{6,2},{1,5},{3,7},{5,1},{7,3},{8,12},{10,14},{12... | collective-permute-start | bytes 208904 | tf_op jit(solution)/shard_map/ppermute | solution.py:489
  17.0 1.1 %collective-permute-start.9 = (s16[272,128]{1,0:T(8,128)(2,1)S(1)}, s16[272,128]{1,0:T(8,128)(2,1)S(1)}, u32[]{:S(2)}, u32[]{:S(2)}) collective-permute-start(s16[272,128]{1,0:T(8,128)(2,1)S(1)} %get-tuple-element.58), channel_id=1, source_target_pairs={{0,6},{2,4},{4,2},{6,0},{1,7},{3,5},{5,3},{7,1},{8,14},{10,12},{12... | collective-permute-start | bytes 208904 | tf_op jit(solution)/shard_map/ppermute | solution.py:489
  18.1 0.0 collective-permute-done.11.refs_1_.refs_2_
  18.1 0.0 collective-permute-done.6.refs_2_.refs_1_.refs_7_
  18.1 0.1 level_states_0.1.refs_3_
  18.3 5.5 %collective-permute-start.17 = (s16[272,128]{1,0:T(8,128)(2,1)S(1)}, s16[272,128]{1,0:T(8,128)(2,1)S(1)}, u32[]{:S(2)}, u32[]{:S(2)}) collective-permute-start(s16[272,128]{1,0:T(8,128)(2,1)S(1)} %level_states_0.1.refs_3_), channel_id=1, source_target_pairs={{0,24},{1,25},{2,26},{3,27},{4,28},{5,29},{6,30},{7,31}} | collective-permute-start | bytes 208904 | tf_op jit(solution)/shard_map/ppermute | solution.py:496
  23.8 1.3 %collective-permute-start.16 = (s16[272,128]{1,0:T(8,128)(2,1)S(1)}, s16[272,128]{1,0:T(8,128)(2,1)S(1)}, u32[]{:S(2)}, u32[]{:S(2)}) collective-permute-start(s16[272,128]{1,0:T(8,128)(2,1)S(1)} %level_states_0.1.refs_3_), channel_id=1, source_target_pairs={{0,16},{8,24},{1,17},{9,25},{2,18},{10,26},{3,19},{11,27},{4,20},{... | collective-permute-start | bytes 208904 | tf_op jit(solution)/shard_map/ppermute | solution.py:496
  25.1 0.0 collective-permute-done.7.refs_2_.refs_1_.refs_8_
  25.1 2.5 %collective-permute-start.15 = (s16[272,128]{1,0:T(8,128)(2,1)S(1)}, s16[272,128]{1,0:T(8,128)(2,1)S(1)}, u32[]{:S(2)}, u32[]{:S(2)}) collective-permute-start(s16[272,128]{1,0:T(8,128)(2,1)S(1)} %level_states_0.1.refs_3_), channel_id=1, source_target_pairs={{0,8},{8,16},{16,24},{1,9},{9,17},{17,25},{2,10},{10,18},{18,26},{... | collective-permute-start | bytes 208904 | tf_op jit(solution)/shard_map/ppermute | solution.py:496
  27.6 0.0 collective-permute-done.8.refs_1_.refs_2_.refs_9_
  27.6 0.0 collective-permute-done.9.refs_0_.refs_3_.refs_10_
  27.6 0.1 level_states_1.1.refs_7_
  27.7 1.3 %collective-permute-start.14 = (s16[272,128]{1,0:T(8,128)(2,1)S(1)}, s16[272,128]{1,0:T(8,128)(2,1)S(1)}, u32[]{:S(2)}, u32[]{:S(2)}) collective-permute-start(s16[272,128]{1,0:T(8,128)(2,1)S(1)} %level_states_1.1.refs_7_), channel_id=1, source_target_pairs={{0,24},{1,25},{2,26},{3,27},{4,28},{5,29},{6,30},{7,31}} | collective-permute-start | bytes 208904 | tf_op jit(solution)/shard_map/ppermute | solution.py:496
  29.0 1.3 %collective-permute-start.13 = (s16[272,128]{1,0:T(8,128)(2,1)S(1)}, s16[272,128]{1,0:T(8,128)(2,1)S(1)}, u32[]{:S(2)}, u32[]{:S(2)}) collective-permute-start(s16[272,128]{1,0:T(8,128)(2,1)S(1)} %level_states_1.1.refs_7_), channel_id=1, source_target_pairs={{0,16},{8,24},{1,17},{9,25},{2,18},{10,26},{3,19},{11,27},{4,20},{... | collective-permute-start | bytes 208904 | tf_op jit(solution)/shard_map/ppermute | solution.py:496
  30.3 0.0 collective-permute-done.17.refs_6_
  30.3 1.3 %collective-permute-start.12 = (s16[272,128]{1,0:T(8,128)(2,1)S(1)}, s16[272,128]{1,0:T(8,128)(2,1)S(1)}, u32[]{:S(2)}, u32[]{:S(2)}) collective-permute-start(s16[272,128]{1,0:T(8,128)(2,1)S(1)} %level_states_1.1.refs_7_), channel_id=1, source_target_pairs={{0,8},{8,16},{16,24},{1,9},{9,17},{17,25},{2,10},{10,18},{18,26},{... | collective-permute-start | bytes 208904 | tf_op jit(solution)/shard_map/ppermute | solution.py:496
  31.6 0.0 collective-permute-done.16.refs_5_
  31.7 0.2 carries_0.1
  31.9 1.8 %collective-permute-start.21 = (s16[272,128]{1,0:T(8,128)(2,1)S(1)}, s16[272,128]{1,0:T(8,128)(2,1)S(1)}, u32[]{:S(2)}, u32[]{:S(2)}) collective-permute-start(s16[272,128]{1,0:T(8,128)(2,1)S(1)} %get-tuple-element.65), channel_id=1, source_target_pairs={{0,6},{2,4},{4,2},{6,0},{1,7},{3,5},{5,3},{7,1},{8,14},{10,12},{12... | collective-permute-start | bytes 208904 | tf_op jit(solution)/shard_map/ppermute | solution.py:489
  33.7 1.0 %collective-permute-start.20 = (s16[272,128]{1,0:T(8,128)(2,1)S(1)}, s16[272,128]{1,0:T(8,128)(2,1)S(1)}, u32[]{:S(2)}, u32[]{:S(2)}) collective-permute-start(s16[272,128]{1,0:T(8,128)(2,1)S(1)} %get-tuple-element.61.refs_7_), channel_id=1, source_target_pairs={{0,2},{2,0},{4,6},{6,4},{1,3},{3,1},{5,7},{7,5},{8,10},{10,8},{12,... | collective-permute-start | bytes 208904 | tf_op jit(solution)/shard_map/ppermute | solution.py:489
  34.7 0.0 collective-permute-done.14.refs_6_.refs_13_
  34.7 0.0 collective-permute-done.13.refs_5_.refs_12_
  34.7 0.0 collective-permute-done.12.refs_4_.refs_11_
  34.7 0.2 carries_1.1
  34.9 1.8 %collective-permute-start.19 = (s16[272,128]{1,0:T(8,128)(2,1)S(1)}, s16[272,128]{1,0:T(8,128)(2,1)S(1)}, u32[]{:S(2)}, u32[]{:S(2)}) collective-permute-start(s16[272,128]{1,0:T(8,128)(2,1)S(1)} %get-tuple-element.63), channel_id=1, source_target_pairs={{0,6},{2,4},{4,2},{6,0},{1,7},{3,5},{5,3},{7,1},{8,14},{10,12},{12... | collective-permute-start | bytes 208904 | tf_op jit(solution)/shard_map/ppermute | solution.py:489
  36.8 0.4 collective-permute-start.18
  37.2 0.0 collective-permute-done.21.refs_9_
  37.2 1.1 %collective-permute-done.20.refs_8_ = s16[272,128]{1,0:T(8,128)(2,1)S(1)} collective-permute-done((s16[272,128]{1,0:T(8,128)(2,1)S(1)}, s16[272,128]{1,0:T(8,128)(2,1)S(1)}, u32[]{:S(2)}, u32[]{:S(2)}) %collective-permute-start.20) | collective-permute-done | bytes 69664 | tf_op jit(solution)/shard_map/ppermute | solution.py:489
  38.3 1.3 %attend_0_1_3.1.refs_10_ = bf16[512,512]{1,0:T(8,128)(2,1)S(1)} custom-call(bf16[256,1024]{1,0:T(8,128)(2,1)S(1)} %get-tuple-element.50.refs_5_.refs_0_, bf16[256,1024]{1,0:T(8,128)(2,1)S(1)} %collective-permute-done.5.refs_5_.refs_4_.refs_1_, bf16[256,1024]{1,0:T(8,128)(2,1)S(1)} %get-tuple-element.46.refs_0_.refs_2_, ...), custom_call_target="tpu_custom_call" | custom-call | flops 402653184 | bytes 2097152 | tf_op jit(solution)/shard_map/attend_0_1_3/pallas_call | solution.py:415
  39.7 1.2 %collective-permute-start.24 = (bf16[512,512]{1,0:T(8,128)(2,1)S(1)}, bf16[512,512]{1,0:T(8,128)(2,1)S(1)}, u32[]{:S(2)}, u32[]{:S(2)}) collective-permute-start(bf16[512,512]{1,0:T(8,128)(2,1)S(1)} %attend_0_1_3.1.refs_10_), channel_id=1, source_target_pairs={{0,2},{2,0},{1,3},{3,1},{4,6},{6,4},{5,7},{7,5},{8,10},{10,8},{9,1... | collective-permute-start | bytes 1572872 | tf_op jit(solution)/shard_map/ppermute | solution.py:489
  40.9 0.0 collective-permute-done.19.refs_9_
  40.9 1.0 %collective-permute-done.18.refs_8_ = s16[272,128]{1,0:T(8,128)(2,1)S(1)} collective-permute-done((s16[272,128]{1,0:T(8,128)(2,1)S(1)}, s16[272,128]{1,0:T(8,128)(2,1)S(1)}, u32[]{:S(2)}, u32[]{:S(2)}) %collective-permute-start.18) | collective-permute-done | bytes 69664 | tf_op jit(solution)/shard_map/ppermute | solution.py:489
  41.9 1.3 %attend_1_1_3.1.refs_14_.refs_10_ = bf16[512,512]{1,0:T(8,128)(2,1)S(1)} custom-call(bf16[256,1024]{1,0:T(8,128)(2,1)S(1)} %get-tuple-element.40.refs_0_, bf16[256,1024]{1,0:T(8,128)(2,1)S(1)} %collective-permute-done.refs_6_.refs_5_.refs_1_, bf16[256,1024]{1,0:T(8,128)(2,1)S(1)} %get-tuple-element.42.refs_0_.refs_2_, ...), custom_call_target="tpu_custom_call" | custom-call | flops 402653184 | bytes 2097152 | tf_op jit(solution)/shard_map/attend_1_1_3/pallas_call | solution.py:415
  43.2 1.0 %collective-permute-start.22 = (bf16[512,512]{1,0:T(8,128)(2,1)S(1)}, bf16[512,512]{1,0:T(8,128)(2,1)S(1)}, u32[]{:S(2)}, u32[]{:S(2)}) collective-permute-start(bf16[512,512]{1,0:T(8,128)(2,1)S(1)} %attend_1_1_3.1.refs_14_.refs_10_), channel_id=1, source_target_pairs={{0,2},{2,0},{1,3},{3,1},{4,6},{6,4},{5,7},{7,5},{8,10},{10,8},{9,1... | collective-permute-start | bytes 1572872 | tf_op jit(solution)/shard_map/ppermute | solution.py:489
  44.2 0.6 own_carries.1
  44.8 1.4 %collective-permute-start.25 = (f32[2,2,128,128]{3,2,1,0:T(8,128)S(1)}, f32[2,2,128,128]{3,2,1,0:T(8,128)S(1)}, u32[]{:S(2)}, u32[]{:S(2)}) collective-permute-start(f32[2,2,128,128]{3,2,1,0:T(8,128)S(1)} %get-tuple-element.69), channel_id=1, source_target_pairs={{0,4},{4,0},{1,5},{5,1},{2,6},{6,2},{3,7},{7,3},{8,12},{12,8},{9,1... | collective-permute-start | bytes 786440 | tf_op jit(solution)/shard_map/ppermute | solution.py:489
  46.2 0.7 %collective-permute-start.23 = (s16[528,128]{1,0:T(8,128)(2,1)S(1)}, s16[528,128]{1,0:T(8,128)(2,1)S(1)}, u32[]{:S(2)}, u32[]{:S(2)}) collective-permute-start(s16[528,128]{1,0:T(8,128)(2,1)S(1)} %get-tuple-element.67), channel_id=1, source_target_pairs={{0,4},{2,6},{4,0},{6,2},{1,5},{3,7},{5,1},{7,3},{8,12},{10,14},{12... | collective-permute-start | bytes 405512 | tf_op jit(solution)/shard_map/ppermute | solution.py:489
  46.9 5.8 %collective-permute-done.23.refs_9_ = s16[528,128]{1,0:T(8,128)(2,1)S(1)} collective-permute-done((s16[528,128]{1,0:T(8,128)(2,1)S(1)}, s16[528,128]{1,0:T(8,128)(2,1)S(1)}, u32[]{:S(2)}, u32[]{:S(2)}) %collective-permute-start.23) | collective-permute-done | bytes 135200 | tf_op jit(solution)/shard_map/ppermute | solution.py:489
  52.7 1.3 %attend_0_0_2.1.refs_10_.refs_0_ = bf16[512,512]{1,0:T(8,128)(2,1)S(1)} custom-call(bf16[256,1024]{1,0:T(8,128)(2,1)S(1)} %get-tuple-element.50.refs_5_.refs_0_, bf16[256,1024]{1,0:T(8,128)(2,1)S(1)} %collective-permute-done.5.refs_5_.refs_4_.refs_1_, bf16[256,1024]{1,0:T(8,128)(2,1)S(1)} %get-tuple-element.46.refs_0_.refs_2_, ...), custom_call_target="tpu_custom_call" | custom-call | flops 402653184 | bytes 2097152 | tf_op jit(solution)/shard_map/attend_0_0_2/pallas_call | solution.py:415
  54.0 1.3 %attend_1_0_2.1.refs_1_ = bf16[512,512]{1,0:T(8,128)(2,1)S(1)} custom-call(bf16[256,1024]{1,0:T(8,128)(2,1)S(1)} %get-tuple-element.40.refs_0_, bf16[256,1024]{1,0:T(8,128)(2,1)S(1)} %collective-permute-done.refs_6_.refs_5_.refs_1_, bf16[256,1024]{1,0:T(8,128)(2,1)S(1)} %get-tuple-element.42.refs_0_.refs_2_, ...), custom_call_target="tpu_custom_call" | custom-call | flops 402653184 | bytes 2097152 | tf_op jit(solution)/shard_map/attend_1_0_2/pallas_call | solution.py:415
  55.4 0.8 %assemble_cache.1 = f32[1,8,128,128]{3,2,1,0:T(8,128)} custom-call(f32[2,2,128,128]{3,2,1,0:T(8,128)S(1)} %get-tuple-element.68.refs_0_, f32[2,2,128,128]{3,2,1,0:T(8,128)S(1)} %collective-permute-done.25.refs_1_), custom_call_target="tpu_custom_call" | custom-call | tf_op jit(solution)/shard_map/assemble_cache/pallas_call | solution.py:475
  56.2 0.0 collective-permute-done.24.refs_2_
  56.2 1.2 %assemble.1.refs_1_ = bf16[1024,1024]{1,0:T(8,128)(2,1)} custom-call(bf16[512,512]{1,0:T(8,128)(2,1)S(1)} %attend_0_0_2.1.refs_10_.refs_0_, bf16[512,512]{1,0:T(8,128)(2,1)S(1)} %attend_1_0_2.1.refs_1_, bf16[512,512]{1,0:T(8,128)(2,1)S(1)} %collective-permute-done.24.refs_2_), custom_call_target="tpu_custom_call" | custom-call | tf_op jit(solution)/shard_map/assemble/pallas_call | solution.py:454
  57.4 5.0 %collective-permute-done.22.refs_0_ = bf16[512,512]{1,0:T(8,128)(2,1)S(1)} collective-permute-done((bf16[512,512]{1,0:T(8,128)(2,1)S(1)}, bf16[512,512]{1,0:T(8,128)(2,1)S(1)}, u32[]{:S(2)}, u32[]{:S(2)}) %collective-permute-start.22) | collective-permute-done | bytes 524320 | tf_op jit(solution)/shard_map/ppermute | solution.py:489
  62.4 0.8 %finish.1 = bf16[1024,1024]{1,0:T(8,128)(2,1)} custom-call(bf16[512,512]{1,0:T(8,128)(2,1)S(1)} %collective-permute-done.22.refs_0_, bf16[1024,1024]{1,0:T(8,128)(2,1)} %assemble.1.refs_1_), custom_call_target="tpu_custom_call", output_to_operand_aliasing={{}: (1, {})} | custom-call | tf_op jit(solution)/shard_map/finish/pallas_call | solution.py:454
  (8 shorter events, 0.0 us)
Async XLA Ops:
  0.6 4.5 %copy-start = (bf16[256,4096]{1,0:T(8,128)(2,1)S(1)}, bf16[256,4096]{1,0:T(8,128)(2,1)}, u32[]{:S(2)}) copy-start(bf16[256,4096]{1,0:T(8,128)(2,1)} %refs_0_.3) | copy-start | bytes 6291460
  4.5 2.1 %collective-permute-start.3 = (bf16[256,1024]{1,0:T(8,128)(2,1)S(1)}, bf16[256,1024]{1,0:T(8,128)(2,1)S(1)}, u32[]{:S(2)}, u32[]{:S(2)}) collective-permute-start(bf16[256,1024]{1,0:T(8,128)(2,1)S(1)} %get-tuple-element.47), channel_id=1, source_target_pairs={{0,1},{1,0},{2,3},{3,2},{4,5},{5,4},{6,7},{7,6},{8,9},{9,8},{10,11... | collective-permute-start | bytes 1572872 | tf_op jit(solution)/shard_map/ppermute | solution.py:489
  5.1 2.3 %collective-permute-start.4 = (bf16[256,1024]{1,0:T(8,128)(2,1)S(1)}, bf16[256,1024]{1,0:T(8,128)(2,1)S(1)}, u32[]{:S(2)}, u32[]{:S(2)}) collective-permute-start(bf16[256,1024]{1,0:T(8,128)(2,1)S(1)} %get-tuple-element.49), channel_id=1, source_target_pairs={{0,1},{1,0},{2,3},{3,2},{4,5},{5,4},{6,7},{7,6},{8,9},{9,8},{10,11... | collective-permute-start | bytes 1572872 | tf_op jit(solution)/shard_map/ppermute | solution.py:489
  5.1 2.2 %copy-start.1 = (f32[1024]{0:T(1024)S(1)}, f32[1024]{0:T(1024)}, u32[]{:S(2)}) copy-start(f32[1024]{0:T(1024)} %param.9) | copy-start | bytes 12292
  5.4 5.7 %collective-permute-start = (bf16[256,1024]{1,0:T(8,128)(2,1)S(1)}, bf16[256,1024]{1,0:T(8,128)(2,1)S(1)}, u32[]{:S(2)}, u32[]{:S(2)}) collective-permute-start(bf16[256,1024]{1,0:T(8,128)(2,1)S(1)} %get-tuple-element.41), channel_id=1, source_target_pairs={{0,1},{1,0},{2,3},{3,2},{4,5},{5,4},{6,7},{7,6},{8,9},{9,8},{10,11... | collective-permute-start | bytes 1572872 | tf_op jit(solution)/shard_map/ppermute | solution.py:489
  5.9 6.6 %collective-permute-start.5 = (bf16[256,1024]{1,0:T(8,128)(2,1)S(1)}, bf16[256,1024]{1,0:T(8,128)(2,1)S(1)}, u32[]{:S(2)}, u32[]{:S(2)}) collective-permute-start(bf16[256,1024]{1,0:T(8,128)(2,1)S(1)} %get-tuple-element.52), channel_id=1, source_target_pairs={{0,1},{1,0},{2,3},{3,2},{4,5},{5,4},{6,7},{7,6},{8,9},{9,8},{10,11... | collective-permute-start | bytes 1572872 | tf_op jit(solution)/shard_map/ppermute | solution.py:489
  6.0 6.7 %collective-permute-start.1 = (bf16[256,1024]{1,0:T(8,128)(2,1)S(1)}, bf16[256,1024]{1,0:T(8,128)(2,1)S(1)}, u32[]{:S(2)}, u32[]{:S(2)}) collective-permute-start(bf16[256,1024]{1,0:T(8,128)(2,1)S(1)} %get-tuple-element.43), channel_id=1, source_target_pairs={{0,1},{1,0},{2,3},{3,2},{4,5},{5,4},{6,7},{7,6},{8,9},{9,8},{10,11... | collective-permute-start | bytes 1572872 | tf_op jit(solution)/shard_map/ppermute | solution.py:489
  6.6 6.1 %collective-permute-start.2 = (bf16[256,1024]{1,0:T(8,128)(2,1)S(1)}, bf16[256,1024]{1,0:T(8,128)(2,1)S(1)}, u32[]{:S(2)}, u32[]{:S(2)}) collective-permute-start(bf16[256,1024]{1,0:T(8,128)(2,1)S(1)} %get-tuple-element.45), channel_id=1, source_target_pairs={{0,1},{1,0},{2,3},{3,2},{4,5},{5,4},{6,7},{7,6},{8,9},{9,8},{10,11... | collective-permute-start | bytes 1572872 | tf_op jit(solution)/shard_map/ppermute | solution.py:489
  8.2 10.0 %collective-permute-start.6 = (s16[288,128]{1,0:T(8,128)(2,1)S(1)}, s16[288,128]{1,0:T(8,128)(2,1)S(1)}, u32[]{:S(2)}, u32[]{:S(2)}) collective-permute-start(s16[288,128]{1,0:T(8,128)(2,1)S(1)} %get-tuple-element.54), channel_id=1, source_target_pairs={{0,2},{2,0},{4,6},{6,4},{1,3},{3,1},{5,7},{7,5},{8,10},{10,8},{12,... | collective-permute-start | bytes 221192 | tf_op jit(solution)/shard_map/ppermute | solution.py:489
  11.1 5.9 %collective-permute-start.10 = (s16[272,128]{1,0:T(8,128)(2,1)S(1)}, s16[272,128]{1,0:T(8,128)(2,1)S(1)}, u32[]{:S(2)}, u32[]{:S(2)}) collective-permute-start(s16[272,128]{1,0:T(8,128)(2,1)S(1)} %get-tuple-element.59), channel_id=1, source_target_pairs={{0,6},{2,4},{4,2},{6,0},{1,7},{3,5},{5,3},{7,1},{8,14},{10,12},{12... | collective-permute-start | bytes 208904 | tf_op jit(solution)/shard_map/ppermute | solution.py:489
  12.6 5.6 %collective-permute-start.11 = (s16[272,128]{1,0:T(8,128)(2,1)S(1)}, s16[272,128]{1,0:T(8,128)(2,1)S(1)}, u32[]{:S(2)}, u32[]{:S(2)}) collective-permute-start(s16[272,128]{1,0:T(8,128)(2,1)S(1)} %get-tuple-element.60), channel_id=1, source_target_pairs={{0,4},{2,6},{4,0},{6,2},{1,5},{3,7},{5,1},{7,3},{8,12},{10,14},{12... | collective-permute-start | bytes 208904 | tf_op jit(solution)/shard_map/ppermute | solution.py:489
  13.5 11.6 %collective-permute-start.7 = (s16[272,128]{1,0:T(8,128)(2,1)S(1)}, s16[272,128]{1,0:T(8,128)(2,1)S(1)}, u32[]{:S(2)}, u32[]{:S(2)}) collective-permute-start(s16[272,128]{1,0:T(8,128)(2,1)S(1)} %get-tuple-element.56), channel_id=1, source_target_pairs={{0,2},{2,0},{4,6},{6,4},{1,3},{3,1},{5,7},{7,5},{8,10},{10,8},{12,... | collective-permute-start | bytes 208904 | tf_op jit(solution)/shard_map/ppermute | solution.py:489
  15.5 12.0 %collective-permute-start.8 = (s16[272,128]{1,0:T(8,128)(2,1)S(1)}, s16[272,128]{1,0:T(8,128)(2,1)S(1)}, u32[]{:S(2)}, u32[]{:S(2)}) collective-permute-start(s16[272,128]{1,0:T(8,128)(2,1)S(1)} %get-tuple-element.57), channel_id=1, source_target_pairs={{0,4},{2,6},{4,0},{6,2},{1,5},{3,7},{5,1},{7,3},{8,12},{10,14},{12... | collective-permute-start | bytes 208904 | tf_op jit(solution)/shard_map/ppermute | solution.py:489
  17.0 10.6 %collective-permute-start.9 = (s16[272,128]{1,0:T(8,128)(2,1)S(1)}, s16[272,128]{1,0:T(8,128)(2,1)S(1)}, u32[]{:S(2)}, u32[]{:S(2)}) collective-permute-start(s16[272,128]{1,0:T(8,128)(2,1)S(1)} %get-tuple-element.58), channel_id=1, source_target_pairs={{0,6},{2,4},{4,2},{6,0},{1,7},{3,5},{5,3},{7,1},{8,14},{10,12},{12... | collective-permute-start | bytes 208904 | tf_op jit(solution)/shard_map/ppermute | solution.py:489
  18.3 12.0 %collective-permute-start.17 = (s16[272,128]{1,0:T(8,128)(2,1)S(1)}, s16[272,128]{1,0:T(8,128)(2,1)S(1)}, u32[]{:S(2)}, u32[]{:S(2)}) collective-permute-start(s16[272,128]{1,0:T(8,128)(2,1)S(1)} %level_states_0.1.refs_3_), channel_id=1, source_target_pairs={{0,24},{1,25},{2,26},{3,27},{4,28},{5,29},{6,30},{7,31}} | collective-permute-start | bytes 208904 | tf_op jit(solution)/shard_map/ppermute | solution.py:496
  23.8 7.9 %collective-permute-start.16 = (s16[272,128]{1,0:T(8,128)(2,1)S(1)}, s16[272,128]{1,0:T(8,128)(2,1)S(1)}, u32[]{:S(2)}, u32[]{:S(2)}) collective-permute-start(s16[272,128]{1,0:T(8,128)(2,1)S(1)} %level_states_0.1.refs_3_), channel_id=1, source_target_pairs={{0,16},{8,24},{1,17},{9,25},{2,18},{10,26},{3,19},{11,27},{4,20},{... | collective-permute-start | bytes 208904 | tf_op jit(solution)/shard_map/ppermute | solution.py:496
  25.1 6.6 %collective-permute-start.15 = (s16[272,128]{1,0:T(8,128)(2,1)S(1)}, s16[272,128]{1,0:T(8,128)(2,1)S(1)}, u32[]{:S(2)}, u32[]{:S(2)}) collective-permute-start(s16[272,128]{1,0:T(8,128)(2,1)S(1)} %level_states_0.1.refs_3_), channel_id=1, source_target_pairs={{0,8},{8,16},{16,24},{1,9},{9,17},{17,25},{2,10},{10,18},{18,26},{... | collective-permute-start | bytes 208904 | tf_op jit(solution)/shard_map/ppermute | solution.py:496
  27.7 7.0 %collective-permute-start.14 = (s16[272,128]{1,0:T(8,128)(2,1)S(1)}, s16[272,128]{1,0:T(8,128)(2,1)S(1)}, u32[]{:S(2)}, u32[]{:S(2)}) collective-permute-start(s16[272,128]{1,0:T(8,128)(2,1)S(1)} %level_states_1.1.refs_7_), channel_id=1, source_target_pairs={{0,24},{1,25},{2,26},{3,27},{4,28},{5,29},{6,30},{7,31}} | collective-permute-start | bytes 208904 | tf_op jit(solution)/shard_map/ppermute | solution.py:496
  29.0 5.7 %collective-permute-start.13 = (s16[272,128]{1,0:T(8,128)(2,1)S(1)}, s16[272,128]{1,0:T(8,128)(2,1)S(1)}, u32[]{:S(2)}, u32[]{:S(2)}) collective-permute-start(s16[272,128]{1,0:T(8,128)(2,1)S(1)} %level_states_1.1.refs_7_), channel_id=1, source_target_pairs={{0,16},{8,24},{1,17},{9,25},{2,18},{10,26},{3,19},{11,27},{4,20},{... | collective-permute-start | bytes 208904 | tf_op jit(solution)/shard_map/ppermute | solution.py:496
  30.3 4.4 %collective-permute-start.12 = (s16[272,128]{1,0:T(8,128)(2,1)S(1)}, s16[272,128]{1,0:T(8,128)(2,1)S(1)}, u32[]{:S(2)}, u32[]{:S(2)}) collective-permute-start(s16[272,128]{1,0:T(8,128)(2,1)S(1)} %level_states_1.1.refs_7_), channel_id=1, source_target_pairs={{0,8},{8,16},{16,24},{1,9},{9,17},{17,25},{2,10},{10,18},{18,26},{... | collective-permute-start | bytes 208904 | tf_op jit(solution)/shard_map/ppermute | solution.py:496
  31.9 5.3 %collective-permute-start.21 = (s16[272,128]{1,0:T(8,128)(2,1)S(1)}, s16[272,128]{1,0:T(8,128)(2,1)S(1)}, u32[]{:S(2)}, u32[]{:S(2)}) collective-permute-start(s16[272,128]{1,0:T(8,128)(2,1)S(1)} %get-tuple-element.65), channel_id=1, source_target_pairs={{0,6},{2,4},{4,2},{6,0},{1,7},{3,5},{5,3},{7,1},{8,14},{10,12},{12... | collective-permute-start | bytes 208904 | tf_op jit(solution)/shard_map/ppermute | solution.py:489
  33.7 4.6 %collective-permute-start.20 = (s16[272,128]{1,0:T(8,128)(2,1)S(1)}, s16[272,128]{1,0:T(8,128)(2,1)S(1)}, u32[]{:S(2)}, u32[]{:S(2)}) collective-permute-start(s16[272,128]{1,0:T(8,128)(2,1)S(1)} %get-tuple-element.61.refs_7_), channel_id=1, source_target_pairs={{0,2},{2,0},{4,6},{6,4},{1,3},{3,1},{5,7},{7,5},{8,10},{10,8},{12,... | collective-permute-start | bytes 208904 | tf_op jit(solution)/shard_map/ppermute | solution.py:489
  34.9 6.0 %collective-permute-start.19 = (s16[272,128]{1,0:T(8,128)(2,1)S(1)}, s16[272,128]{1,0:T(8,128)(2,1)S(1)}, u32[]{:S(2)}, u32[]{:S(2)}) collective-permute-start(s16[272,128]{1,0:T(8,128)(2,1)S(1)} %get-tuple-element.63), channel_id=1, source_target_pairs={{0,6},{2,4},{4,2},{6,0},{1,7},{3,5},{5,3},{7,1},{8,14},{10,12},{12... | collective-permute-start | bytes 208904 | tf_op jit(solution)/shard_map/ppermute | solution.py:489
  36.8 5.1 %collective-permute-start.18 = (s16[272,128]{1,0:T(8,128)(2,1)S(1)}, s16[272,128]{1,0:T(8,128)(2,1)S(1)}, u32[]{:S(2)}, u32[]{:S(2)}) collective-permute-start(s16[272,128]{1,0:T(8,128)(2,1)S(1)} %get-tuple-element.62.refs_10_), channel_id=1, source_target_pairs={{0,2},{2,0},{4,6},{6,4},{1,3},{3,1},{5,7},{7,5},{8,10},{10,8},{12,... | collective-permute-start | bytes 208904 | tf_op jit(solution)/shard_map/ppermute | solution.py:489
  39.7 16.5 %collective-permute-start.24 = (bf16[512,512]{1,0:T(8,128)(2,1)S(1)}, bf16[512,512]{1,0:T(8,128)(2,1)S(1)}, u32[]{:S(2)}, u32[]{:S(2)}) collective-permute-start(bf16[512,512]{1,0:T(8,128)(2,1)S(1)} %attend_0_1_3.1.refs_10_), channel_id=1, source_target_pairs={{0,2},{2,0},{1,3},{3,1},{4,6},{6,4},{5,7},{7,5},{8,10},{10,8},{9,1... | collective-permute-start | bytes 1572872 | tf_op jit(solution)/shard_map/ppermute | solution.py:489
  43.2 19.2 %collective-permute-start.22 = (bf16[512,512]{1,0:T(8,128)(2,1)S(1)}, bf16[512,512]{1,0:T(8,128)(2,1)S(1)}, u32[]{:S(2)}, u32[]{:S(2)}) collective-permute-start(bf16[512,512]{1,0:T(8,128)(2,1)S(1)} %attend_1_1_3.1.refs_14_.refs_10_), channel_id=1, source_target_pairs={{0,2},{2,0},{1,3},{3,1},{4,6},{6,4},{5,7},{7,5},{8,10},{10,8},{9,1... | collective-permute-start | bytes 1572872 | tf_op jit(solution)/shard_map/ppermute | solution.py:489
  44.8 10.5 %collective-permute-start.25 = (f32[2,2,128,128]{3,2,1,0:T(8,128)S(1)}, f32[2,2,128,128]{3,2,1,0:T(8,128)S(1)}, u32[]{:S(2)}, u32[]{:S(2)}) collective-permute-start(f32[2,2,128,128]{3,2,1,0:T(8,128)S(1)} %get-tuple-element.69), channel_id=1, source_target_pairs={{0,4},{4,0},{1,5},{5,1},{2,6},{6,2},{3,7},{7,3},{8,12},{12,8},{9,1... | collective-permute-start | bytes 786440 | tf_op jit(solution)/shard_map/ppermute | solution.py:489
  46.2 6.5 %collective-permute-start.23 = (s16[528,128]{1,0:T(8,128)(2,1)S(1)}, s16[528,128]{1,0:T(8,128)(2,1)S(1)}, u32[]{:S(2)}, u32[]{:S(2)}) collective-permute-start(s16[528,128]{1,0:T(8,128)(2,1)S(1)} %get-tuple-element.67), channel_id=1, source_target_pairs={{0,4},{2,6},{4,0},{6,2},{1,5},{3,7},{5,1},{7,3},{8,12},{10,14},{12... | collective-permute-start | bytes 405512 | tf_op jit(solution)/shard_map/ppermute | solution.py:489

commit v16 on v15

--- a/solution.py
+++ b/solution.py
@@ -554,7 +554,10 @@
     levels = []
     for half in halves:
         level = level_states(plan, own[half], others[half][::-1], half, after)
-        levels.append([to_later(level, d) for d in range(1, plan.n_outer)])
+        distances = [*range(1, plan.n_outer)]
+        if half == 0:
+            distances = [*distances[1:], *distances[:1]]
+        levels.append([to_later(level, d) for d in distances])
         after = [level]
     carry = []
     for half in halves:

time: 63.6 us -> 63.5 us (level)
  no operation moved by 1% of the time
where the time goes in v16:
time: 63.5 us; the launch traced here: 63.2 us
  starting transfers between devices  33.7 us (53%)
  Pallas kernels  15.1 us (24%)
  waiting for transfers between devices  13.5 us (21%)
  between operations  0.85 us (1%)
    ppermute x20, starting transfers between devices, swap(): return lax.ppermute(array, axes, [(i, i ^ offset) for i in range(size)])  20.5 us
    ppermute x20, waiting for transfers between devices, swap(): return lax.ppermute(array, axes, [(i, i ^ offset) for i in range(size)])  13.5 us
    ppermute x6, starting transfers between devices, to_later(): return lax.ppermute(array, 'outer', pairs)  13.2 us
    pallas_call x4, Pallas kernels, attend(): pl.pallas_call(at_place(kernel), out_shape=jax.ShapeDtypeStruct((CORES *...  5.29 us
    pallas_call x1, Pallas kernels, decode(): pl.pallas_call(kernel, out_shape=[jax.ShapeDtypeStruct((rows, plan.n_y *...  3.88 us
    pallas_call x2, Pallas kernels, assemble(): pl.pallas_call(at_place(kernel), out_shape=jax.ShapeDtypeStruct((plan.n_y...  1.99 us
    pallas_call x2, Pallas kernels, chunk_states(): pl.pallas_call(at_place(kernel), out_shape=[states_shape(plan.each), stat...  1.64 us
  transfers between devices with their start and end apart: 26, of which 6 were waited for; matrix products, arithmetic and copies ran while one was open for 0% of the time, Pallas kernels for 17%

profile of v16, /device:TPU:0, one launch (start us, length us, event | category | flops | bytes accessed | tf_op | source)
XLA Modules:
  0.0 63.2 jit_solution(15404802746299196745)
XLA Ops:
  0.6 3.9 %decode.1 = (bf16[256,1024]{1,0:T(8,128)(2,1)S(1)}, bf16[256,1024]{1,0:T(8,128)(2,1)S(1)}, bf16[256,1024]{1,0:T(8,128)(2,1)S(1)}, bf16[256,1024]{1,0:T(8,128)(2,...) custom-call(s32[256,4096]{1,0:T(8,128)} %refs_0_.2, ...), custom_call_target="tpu_custom_call" | custom-call | flops 4194304 | bytes 14680064 | tf_op jit(solution)/shard_map/decode/pallas_call | solution.py:114
  4.5 0.5 collective-permute-start.3
  5.1 0.1 collective-permute-start.4
  5.1 0.3 spike_queries.1
  5.4 0.5 collective-permute-start
  5.9 0.1 collective-permute-start.5
  6.0 0.4 collective-permute-start.1
  6.4 0.2 collective-permute-done.3.refs_1_.refs_3_
  6.6 0.4 collective-permute-start.2
  7.0 0.4 collective-permute-done.4.refs_3_.refs_5_
  7.3 0.8 %chunk_states_0.1 = (f32[2,128,128]{2,1,0:T(8,128)S(1)}, f32[4,2,128,128]{3,2,1,0:T(8,128)S(1)}, s16[288,128]{1,0:T(8,128)(2,1)S(1)}, s16[272,128]{1,0:T(8,128)(2,1)S(1)}, s16[272,128]{1,0:T(8,128)(2,1)S(1)}) custom-call(bf16[256,1024]{1,0:T(8,128)(2,1)S(1)} %get-tuple-element.46.refs_0_.refs_2_, ...), custom_call_target="tpu_custom_call" | custom-call | flops 134217728 | bytes 2883584 | tf_op jit(solution)/shard_map/chunk_states_0/pallas_call | solution.py:251
  8.2 3.0 %collective-permute-start.6 = (s16[288,128]{1,0:T(8,128)(2,1)S(1)}, s16[288,128]{1,0:T(8,128)(2,1)S(1)}, u32[]{:S(2)}, u32[]{:S(2)}) collective-permute-start(s16[288,128]{1,0:T(8,128)(2,1)S(1)} %get-tuple-element.54), channel_id=1, source_target_pairs={{0,2},{2,0},{4,6},{6,4},{1,3},{3,1},{5,7},{7,5},{8,10},{10,8},{12,... | collective-permute-start | bytes 221192 | tf_op jit(solution)/shard_map/ppermute | solution.py:489
  11.1 0.0 collective-permute-done.refs_6_.refs_5_.refs_1_
  11.1 1.4 %collective-permute-start.10 = (s16[272,128]{1,0:T(8,128)(2,1)S(1)}, s16[272,128]{1,0:T(8,128)(2,1)S(1)}, u32[]{:S(2)}, u32[]{:S(2)}) collective-permute-start(s16[272,128]{1,0:T(8,128)(2,1)S(1)} %get-tuple-element.59), channel_id=1, source_target_pairs={{0,6},{2,4},{4,2},{6,0},{1,7},{3,5},{5,3},{7,1},{8,14},{10,12},{12... | collective-permute-start | bytes 208904 | tf_op jit(solution)/shard_map/ppermute | solution.py:489
  12.6 0.0 collective-permute-done.5.refs_5_.refs_4_.refs_1_
  12.6 0.1 collective-permute-start.11
  12.7 0.0 collective-permute-done.1.refs_1_.refs_3_
  12.7 0.0 collective-permute-done.2.refs_3_.refs_5_
  12.7 0.8 %chunk_states_1.1 = (f32[2,128,128]{2,1,0:T(8,128)S(1)}, f32[4,2,128,128]{3,2,1,0:T(8,128)S(1)}, s16[272,128]{1,0:T(8,128)(2,1)S(1)}, s16[272,128]{1,0:T(8,128)(2,1)S(1)}, s16[272,128]{1,0:T(8,128)(2,1)S(1)}) custom-call(bf16[256,1024]{1,0:T(8,128)(2,1)S(1)} %get-tuple-element.42.refs_0_.refs_2_, ...), custom_call_target="tpu_custom_call" | custom-call | flops 134217728 | bytes 2883584 | tf_op jit(solution)/shard_map/chunk_states_1/pallas_call | solution.py:251
  13.5 2.0 %collective-permute-start.7 = (s16[272,128]{1,0:T(8,128)(2,1)S(1)}, s16[272,128]{1,0:T(8,128)(2,1)S(1)}, u32[]{:S(2)}, u32[]{:S(2)}) collective-permute-start(s16[272,128]{1,0:T(8,128)(2,1)S(1)} %get-tuple-element.56), channel_id=1, source_target_pairs={{0,2},{2,0},{4,6},{6,4},{1,3},{3,1},{5,7},{7,5},{8,10},{10,8},{12,... | collective-permute-start | bytes 208904 | tf_op jit(solution)/shard_map/ppermute | solution.py:489
  15.5 1.5 %collective-permute-start.8 = (s16[272,128]{1,0:T(8,128)(2,1)S(1)}, s16[272,128]{1,0:T(8,128)(2,1)S(1)}, u32[]{:S(2)}, u32[]{:S(2)}) collective-permute-start(s16[272,128]{1,0:T(8,128)(2,1)S(1)} %get-tuple-element.57), channel_id=1, source_target_pairs={{0,4},{2,6},{4,0},{6,2},{1,5},{3,7},{5,1},{7,3},{8,12},{10,14},{12... | collective-permute-start | bytes 208904 | tf_op jit(solution)/shard_map/ppermute | solution.py:489
  17.0 0.0 collective-permute-done.10.refs_0_.refs_3_
  17.0 1.1 %collective-permute-start.9 = (s16[272,128]{1,0:T(8,128)(2,1)S(1)}, s16[272,128]{1,0:T(8,128)(2,1)S(1)}, u32[]{:S(2)}, u32[]{:S(2)}) collective-permute-start(s16[272,128]{1,0:T(8,128)(2,1)S(1)} %get-tuple-element.58), channel_id=1, source_target_pairs={{0,6},{2,4},{4,2},{6,0},{1,7},{3,5},{5,3},{7,1},{8,14},{10,12},{12... | collective-permute-start | bytes 208904 | tf_op jit(solution)/shard_map/ppermute | solution.py:489
  18.1 0.0 collective-permute-done.11.refs_1_.refs_2_
  18.1 0.0 collective-permute-done.6.refs_2_.refs_1_.refs_7_
  18.1 0.1 level_states_0.1.refs_3_
  18.3 3.5 %collective-permute-start.17 = (s16[272,128]{1,0:T(8,128)(2,1)S(1)}, s16[272,128]{1,0:T(8,128)(2,1)S(1)}, u32[]{:S(2)}, u32[]{:S(2)}) collective-permute-start(s16[272,128]{1,0:T(8,128)(2,1)S(1)} %level_states_0.1.refs_3_), channel_id=1, source_target_pairs={{0,8},{8,16},{16,24},{1,9},{9,17},{17,25},{2,10},{10,18},{18,26},{... | collective-permute-start | bytes 208904 | tf_op jit(solution)/shard_map/ppermute | solution.py:496
  21.7 3.3 %collective-permute-start.16 = (s16[272,128]{1,0:T(8,128)(2,1)S(1)}, s16[272,128]{1,0:T(8,128)(2,1)S(1)}, u32[]{:S(2)}, u32[]{:S(2)}) collective-permute-start(s16[272,128]{1,0:T(8,128)(2,1)S(1)} %level_states_0.1.refs_3_), channel_id=1, source_target_pairs={{0,24},{1,25},{2,26},{3,27},{4,28},{5,29},{6,30},{7,31}} | collective-permute-start | bytes 208904 | tf_op jit(solution)/shard_map/ppermute | solution.py:496
  25.1 0.0 collective-permute-done.7.refs_2_.refs_1_.refs_8_
  25.1 1.8 %collective-permute-start.15 = (s16[272,128]{1,0:T(8,128)(2,1)S(1)}, s16[272,128]{1,0:T(8,128)(2,1)S(1)}, u32[]{:S(2)}, u32[]{:S(2)}) collective-permute-start(s16[272,128]{1,0:T(8,128)(2,1)S(1)} %level_states_0.1.refs_3_), channel_id=1, source_target_pairs={{0,16},{8,24},{1,17},{9,25},{2,18},{10,26},{3,19},{11,27},{4,20},{... | collective-permute-start | bytes 208904 | tf_op jit(solution)/shard_map/ppermute | solution.py:496
  26.9 0.0 collective-permute-done.8.refs_1_.refs_2_.refs_9_
  26.9 0.0 collective-permute-done.9.refs_0_.refs_3_.refs_10_
  27.0 0.1 level_states_1.1.refs_7_
  27.1 1.3 %collective-permute-start.14 = (s16[272,128]{1,0:T(8,128)(2,1)S(1)}, s16[272,128]{1,0:T(8,128)(2,1)S(1)}, u32[]{:S(2)}, u32[]{:S(2)}) collective-permute-start(s16[272,128]{1,0:T(8,128)(2,1)S(1)} %level_states_1.1.refs_7_), channel_id=1, source_target_pairs={{0,24},{1,25},{2,26},{3,27},{4,28},{5,29},{6,30},{7,31}} | collective-permute-start | bytes 208904 | tf_op jit(solution)/shard_map/ppermute | solution.py:496
  28.4 1.3 %collective-permute-start.13 = (s16[272,128]{1,0:T(8,128)(2,1)S(1)}, s16[272,128]{1,0:T(8,128)(2,1)S(1)}, u32[]{:S(2)}, u32[]{:S(2)}) collective-permute-start(s16[272,128]{1,0:T(8,128)(2,1)S(1)} %level_states_1.1.refs_7_), channel_id=1, source_target_pairs={{0,16},{8,24},{1,17},{9,25},{2,18},{10,26},{3,19},{11,27},{4,20},{... | collective-permute-start | bytes 208904 | tf_op jit(solution)/shard_map/ppermute | solution.py:496
  29.7 0.0 collective-permute-done.17.refs_6_
  29.7 2.0 %collective-permute-start.12 = (s16[272,128]{1,0:T(8,128)(2,1)S(1)}, s16[272,128]{1,0:T(8,128)(2,1)S(1)}, u32[]{:S(2)}, u32[]{:S(2)}) collective-permute-start(s16[272,128]{1,0:T(8,128)(2,1)S(1)} %level_states_1.1.refs_7_), channel_id=1, source_target_pairs={{0,8},{8,16},{16,24},{1,9},{9,17},{17,25},{2,10},{10,18},{18,26},{... | collective-permute-start | bytes 208904 | tf_op jit(solution)/shard_map/ppermute | solution.py:496
  31.6 0.0 collective-permute-done.16.refs_5_
  31.7 0.0 collective-permute-done.15.refs_4_
  31.7 0.2 carries_0.1
  31.9 1.8 %collective-permute-start.21 = (s16[272,128]{1,0:T(8,128)(2,1)S(1)}, s16[272,128]{1,0:T(8,128)(2,1)S(1)}, u32[]{:S(2)}, u32[]{:S(2)}) collective-permute-start(s16[272,128]{1,0:T(8,128)(2,1)S(1)} %get-tuple-element.65), channel_id=1, source_target_pairs={{0,6},{2,4},{4,2},{6,0},{1,7},{3,5},{5,3},{7,1},{8,14},{10,12},{12... | collective-permute-start | bytes 208904 | tf_op jit(solution)/shard_map/ppermute | solution.py:489
  33.7 1.0 %collective-permute-start.20 = (s16[272,128]{1,0:T(8,128)(2,1)S(1)}, s16[272,128]{1,0:T(8,128)(2,1)S(1)}, u32[]{:S(2)}, u32[]{:S(2)}) collective-permute-start(s16[272,128]{1,0:T(8,128)(2,1)S(1)} %get-tuple-element.61.refs_7_), channel_id=1, source_target_pairs={{0,2},{2,0},{4,6},{6,4},{1,3},{3,1},{5,7},{7,5},{8,10},{10,8},{12,... | collective-permute-start | bytes 208904 | tf_op jit(solution)/shard_map/ppermute | solution.py:489
  34.7 0.0 collective-permute-done.14.refs_6_.refs_13_
  34.7 0.2 carries_1.1
  34.9 1.8 %collective-permute-start.19 = (s16[272,128]{1,0:T(8,128)(2,1)S(1)}, s16[272,128]{1,0:T(8,128)(2,1)S(1)}, u32[]{:S(2)}, u32[]{:S(2)}) collective-permute-start(s16[272,128]{1,0:T(8,128)(2,1)S(1)} %get-tuple-element.63), channel_id=1, source_target_pairs={{0,6},{2,4},{4,2},{6,0},{1,7},{3,5},{5,3},{7,1},{8,14},{10,12},{12... | collective-permute-start | bytes 208904 | tf_op jit(solution)/shard_map/ppermute | solution.py:489
  36.7 0.4 collective-permute-start.18
  37.2 0.0 collective-permute-done.21.refs_9_
  37.2 1.1 %collective-permute-done.20.refs_8_ = s16[272,128]{1,0:T(8,128)(2,1)S(1)} collective-permute-done((s16[272,128]{1,0:T(8,128)(2,1)S(1)}, s16[272,128]{1,0:T(8,128)(2,1)S(1)}, u32[]{:S(2)}, u32[]{:S(2)}) %collective-permute-start.20) | collective-permute-done | bytes 69664 | tf_op jit(solution)/shard_map/ppermute | solution.py:489
  38.3 1.3 %attend_0_1_3.1.refs_10_ = bf16[512,512]{1,0:T(8,128)(2,1)S(1)} custom-call(bf16[256,1024]{1,0:T(8,128)(2,1)S(1)} %get-tuple-element.50.refs_5_.refs_0_, bf16[256,1024]{1,0:T(8,128)(2,1)S(1)} %collective-permute-done.5.refs_5_.refs_4_.refs_1_, bf16[256,1024]{1,0:T(8,128)(2,1)S(1)} %get-tuple-element.46.refs_0_.refs_2_, ...), custom_call_target="tpu_custom_call" | custom-call | flops 402653184 | bytes 2097152 | tf_op jit(solution)/shard_map/attend_0_1_3/pallas_call | solution.py:415
  39.7 1.2 %collective-permute-start.24 = (bf16[512,512]{1,0:T(8,128)(2,1)S(1)}, bf16[512,512]{1,0:T(8,128)(2,1)S(1)}, u32[]{:S(2)}, u32[]{:S(2)}) collective-permute-start(bf16[512,512]{1,0:T(8,128)(2,1)S(1)} %attend_0_1_3.1.refs_10_), channel_id=1, source_target_pairs={{0,2},{2,0},{1,3},{3,1},{4,6},{6,4},{5,7},{7,5},{8,10},{10,8},{9,1... | collective-permute-start | bytes 1572872 | tf_op jit(solution)/shard_map/ppermute | solution.py:489
  40.9 1.0 %collective-permute-done.18.refs_8_ = s16[272,128]{1,0:T(8,128)(2,1)S(1)} collective-permute-done((s16[272,128]{1,0:T(8,128)(2,1)S(1)}, s16[272,128]{1,0:T(8,128)(2,1)S(1)}, u32[]{:S(2)}, u32[]{:S(2)}) %collective-permute-start.18) | collective-permute-done | bytes 69664 | tf_op jit(solution)/shard_map/ppermute | solution.py:489
  41.9 1.3 %attend_1_1_3.1.refs_14_.refs_10_ = bf16[512,512]{1,0:T(8,128)(2,1)S(1)} custom-call(bf16[256,1024]{1,0:T(8,128)(2,1)S(1)} %get-tuple-element.40.refs_0_, bf16[256,1024]{1,0:T(8,128)(2,1)S(1)} %collective-permute-done.refs_6_.refs_5_.refs_1_, bf16[256,1024]{1,0:T(8,128)(2,1)S(1)} %get-tuple-element.42.refs_0_.refs_2_, ...), custom_call_target="tpu_custom_call" | custom-call | flops 402653184 | bytes 2097152 | tf_op jit(solution)/shard_map/attend_1_1_3/pallas_call | solution.py:415
  43.2 1.0 %collective-permute-start.22 = (bf16[512,512]{1,0:T(8,128)(2,1)S(1)}, bf16[512,512]{1,0:T(8,128)(2,1)S(1)}, u32[]{:S(2)}, u32[]{:S(2)}) collective-permute-start(bf16[512,512]{1,0:T(8,128)(2,1)S(1)} %attend_1_1_3.1.refs_14_.refs_10_), channel_id=1, source_target_pairs={{0,2},{2,0},{1,3},{3,1},{4,6},{6,4},{5,7},{7,5},{8,10},{10,8},{9,1... | collective-permute-start | bytes 1572872 | tf_op jit(solution)/shard_map/ppermute | solution.py:489
  44.2 0.6 own_carries.1
  44.8 1.4 %collective-permute-start.25 = (f32[2,2,128,128]{3,2,1,0:T(8,128)S(1)}, f32[2,2,128,128]{3,2,1,0:T(8,128)S(1)}, u32[]{:S(2)}, u32[]{:S(2)}) collective-permute-start(f32[2,2,128,128]{3,2,1,0:T(8,128)S(1)} %get-tuple-element.69), channel_id=1, source_target_pairs={{0,4},{4,0},{1,5},{5,1},{2,6},{6,2},{3,7},{7,3},{8,12},{12,8},{9,1... | collective-permute-start | bytes 786440 | tf_op jit(solution)/shard_map/ppermute | solution.py:489
  46.2 0.7 %collective-permute-start.23 = (s16[528,128]{1,0:T(8,128)(2,1)S(1)}, s16[528,128]{1,0:T(8,128)(2,1)S(1)}, u32[]{:S(2)}, u32[]{:S(2)}) collective-permute-start(s16[528,128]{1,0:T(8,128)(2,1)S(1)} %get-tuple-element.67), channel_id=1, source_target_pairs={{0,4},{2,6},{4,0},{6,2},{1,5},{3,7},{5,1},{7,3},{8,12},{10,14},{12... | collective-permute-start | bytes 405512 | tf_op jit(solution)/shard_map/ppermute | solution.py:489
  46.9 5.8 %collective-permute-done.23.refs_9_ = s16[528,128]{1,0:T(8,128)(2,1)S(1)} collective-permute-done((s16[528,128]{1,0:T(8,128)(2,1)S(1)}, s16[528,128]{1,0:T(8,128)(2,1)S(1)}, u32[]{:S(2)}, u32[]{:S(2)}) %collective-permute-start.23) | collective-permute-done | bytes 135200 | tf_op jit(solution)/shard_map/ppermute | solution.py:489
  52.7 1.3 %attend_0_0_2.1.refs_10_.refs_0_ = bf16[512,512]{1,0:T(8,128)(2,1)S(1)} custom-call(bf16[256,1024]{1,0:T(8,128)(2,1)S(1)} %get-tuple-element.50.refs_5_.refs_0_, bf16[256,1024]{1,0:T(8,128)(2,1)S(1)} %collective-permute-done.5.refs_5_.refs_4_.refs_1_, bf16[256,1024]{1,0:T(8,128)(2,1)S(1)} %get-tuple-element.46.refs_0_.refs_2_, ...), custom_call_target="tpu_custom_call" | custom-call | flops 402653184 | bytes 2097152 | tf_op jit(solution)/shard_map/attend_0_0_2/pallas_call | solution.py:415
  54.0 1.3 %attend_1_0_2.1.refs_1_ = bf16[512,512]{1,0:T(8,128)(2,1)S(1)} custom-call(bf16[256,1024]{1,0:T(8,128)(2,1)S(1)} %get-tuple-element.40.refs_0_, bf16[256,1024]{1,0:T(8,128)(2,1)S(1)} %collective-permute-done.refs_6_.refs_5_.refs_1_, bf16[256,1024]{1,0:T(8,128)(2,1)S(1)} %get-tuple-element.42.refs_0_.refs_2_, ...), custom_call_target="tpu_custom_call" | custom-call | flops 402653184 | bytes 2097152 | tf_op jit(solution)/shard_map/attend_1_0_2/pallas_call | solution.py:415
  55.3 0.0 collective-permute-done.25.refs_1_
  55.4 0.8 %assemble_cache.1 = f32[1,8,128,128]{3,2,1,0:T(8,128)} custom-call(f32[2,2,128,128]{3,2,1,0:T(8,128)S(1)} %get-tuple-element.68.refs_0_, f32[2,2,128,128]{3,2,1,0:T(8,128)S(1)} %collective-permute-done.25.refs_1_), custom_call_target="tpu_custom_call" | custom-call | tf_op jit(solution)/shard_map/assemble_cache/pallas_call | solution.py:475
  56.2 1.2 %assemble.1.refs_1_ = bf16[1024,1024]{1,0:T(8,128)(2,1)} custom-call(bf16[512,512]{1,0:T(8,128)(2,1)S(1)} %attend_0_0_2.1.refs_10_.refs_0_, bf16[512,512]{1,0:T(8,128)(2,1)S(1)} %attend_1_0_2.1.refs_1_, bf16[512,512]{1,0:T(8,128)(2,1)S(1)} %collective-permute-done.24.refs_2_), custom_call_target="tpu_custom_call" | custom-call | tf_op jit(solution)/shard_map/assemble/pallas_call | solution.py:454
  57.4 5.0 %collective-permute-done.22.refs_0_ = bf16[512,512]{1,0:T(8,128)(2,1)S(1)} collective-permute-done((bf16[512,512]{1,0:T(8,128)(2,1)S(1)}, bf16[512,512]{1,0:T(8,128)(2,1)S(1)}, u32[]{:S(2)}, u32[]{:S(2)}) %collective-permute-start.22) | collective-permute-done | bytes 524320 | tf_op jit(solution)/shard_map/ppermute | solution.py:489
  62.4 0.8 %finish.1 = bf16[1024,1024]{1,0:T(8,128)(2,1)} custom-call(bf16[512,512]{1,0:T(8,128)(2,1)S(1)} %collective-permute-done.22.refs_0_, bf16[1024,1024]{1,0:T(8,128)(2,1)} %assemble.1.refs_1_), custom_call_target="tpu_custom_call", output_to_operand_aliasing={{}: (1, {})} | custom-call | tf_op jit(solution)/shard_map/finish/pallas_call | solution.py:454
  (8 shorter events, 0.0 us)
Async XLA Ops:
  0.6 4.5 %copy-start = (bf16[256,4096]{1,0:T(8,128)(2,1)S(1)}, bf16[256,4096]{1,0:T(8,128)(2,1)}, u32[]{:S(2)}) copy-start(bf16[256,4096]{1,0:T(8,128)(2,1)} %refs_0_.3) | copy-start | bytes 6291460
  4.5 2.1 %collective-permute-start.3 = (bf16[256,1024]{1,0:T(8,128)(2,1)S(1)}, bf16[256,1024]{1,0:T(8,128)(2,1)S(1)}, u32[]{:S(2)}, u32[]{:S(2)}) collective-permute-start(bf16[256,1024]{1,0:T(8,128)(2,1)S(1)} %get-tuple-element.47), channel_id=1, source_target_pairs={{0,1},{1,0},{2,3},{3,2},{4,5},{5,4},{6,7},{7,6},{8,9},{9,8},{10,11... | collective-permute-start | bytes 1572872 | tf_op jit(solution)/shard_map/ppermute | solution.py:489
  5.1 2.3 %collective-permute-start.4 = (bf16[256,1024]{1,0:T(8,128)(2,1)S(1)}, bf16[256,1024]{1,0:T(8,128)(2,1)S(1)}, u32[]{:S(2)}, u32[]{:S(2)}) collective-permute-start(bf16[256,1024]{1,0:T(8,128)(2,1)S(1)} %get-tuple-element.49), channel_id=1, source_target_pairs={{0,1},{1,0},{2,3},{3,2},{4,5},{5,4},{6,7},{7,6},{8,9},{9,8},{10,11... | collective-permute-start | bytes 1572872 | tf_op jit(solution)/shard_map/ppermute | solution.py:489
  5.1 2.2 %copy-start.1 = (f32[1024]{0:T(1024)S(1)}, f32[1024]{0:T(1024)}, u32[]{:S(2)}) copy-start(f32[1024]{0:T(1024)} %param.9) | copy-start | bytes 12292
  5.4 5.7 %collective-permute-start = (bf16[256,1024]{1,0:T(8,128)(2,1)S(1)}, bf16[256,1024]{1,0:T(8,128)(2,1)S(1)}, u32[]{:S(2)}, u32[]{:S(2)}) collective-permute-start(bf16[256,1024]{1,0:T(8,128)(2,1)S(1)} %get-tuple-element.41), channel_id=1, source_target_pairs={{0,1},{1,0},{2,3},{3,2},{4,5},{5,4},{6,7},{7,6},{8,9},{9,8},{10,11... | collective-permute-start | bytes 1572872 | tf_op jit(solution)/shard_map/ppermute | solution.py:489
  5.9 6.6 %collective-permute-start.5 = (bf16[256,1024]{1,0:T(8,128)(2,1)S(1)}, bf16[256,1024]{1,0:T(8,128)(2,1)S(1)}, u32[]{:S(2)}, u32[]{:S(2)}) collective-permute-start(bf16[256,1024]{1,0:T(8,128)(2,1)S(1)} %get-tuple-element.52), channel_id=1, source_target_pairs={{0,1},{1,0},{2,3},{3,2},{4,5},{5,4},{6,7},{7,6},{8,9},{9,8},{10,11... | collective-permute-start | bytes 1572872 | tf_op jit(solution)/shard_map/ppermute | solution.py:489
  6.0 6.7 %collective-permute-start.1 = (bf16[256,1024]{1,0:T(8,128)(2,1)S(1)}, bf16[256,1024]{1,0:T(8,128)(2,1)S(1)}, u32[]{:S(2)}, u32[]{:S(2)}) collective-permute-start(bf16[256,1024]{1,0:T(8,128)(2,1)S(1)} %get-tuple-element.43), channel_id=1, source_target_pairs={{0,1},{1,0},{2,3},{3,2},{4,5},{5,4},{6,7},{7,6},{8,9},{9,8},{10,11... | collective-permute-start | bytes 1572872 | tf_op jit(solution)/shard_map/ppermute | solution.py:489
  6.6 6.1 %collective-permute-start.2 = (bf16[256,1024]{1,0:T(8,128)(2,1)S(1)}, bf16[256,1024]{1,0:T(8,128)(2,1)S(1)}, u32[]{:S(2)}, u32[]{:S(2)}) collective-permute-start(bf16[256,1024]{1,0:T(8,128)(2,1)S(1)} %get-tuple-element.45), channel_id=1, source_target_pairs={{0,1},{1,0},{2,3},{3,2},{4,5},{5,4},{6,7},{7,6},{8,9},{9,8},{10,11... | collective-permute-start | bytes 1572872 | tf_op jit(solution)/shard_map/ppermute | solution.py:489
  8.2 10.0 %collective-permute-start.6 = (s16[288,128]{1,0:T(8,128)(2,1)S(1)}, s16[288,128]{1,0:T(8,128)(2,1)S(1)}, u32[]{:S(2)}, u32[]{:S(2)}) collective-permute-start(s16[288,128]{1,0:T(8,128)(2,1)S(1)} %get-tuple-element.54), channel_id=1, source_target_pairs={{0,2},{2,0},{4,6},{6,4},{1,3},{3,1},{5,7},{7,5},{8,10},{10,8},{12,... | collective-permute-start | bytes 221192 | tf_op jit(solution)/shard_map/ppermute | solution.py:489
  11.1 5.9 %collective-permute-start.10 = (s16[272,128]{1,0:T(8,128)(2,1)S(1)}, s16[272,128]{1,0:T(8,128)(2,1)S(1)}, u32[]{:S(2)}, u32[]{:S(2)}) collective-permute-start(s16[272,128]{1,0:T(8,128)(2,1)S(1)} %get-tuple-element.59), channel_id=1, source_target_pairs={{0,6},{2,4},{4,2},{6,0},{1,7},{3,5},{5,3},{7,1},{8,14},{10,12},{12... | collective-permute-start | bytes 208904 | tf_op jit(solution)/shard_map/ppermute | solution.py:489
  12.6 5.6 %collective-permute-start.11 = (s16[272,128]{1,0:T(8,128)(2,1)S(1)}, s16[272,128]{1,0:T(8,128)(2,1)S(1)}, u32[]{:S(2)}, u32[]{:S(2)}) collective-permute-start(s16[272,128]{1,0:T(8,128)(2,1)S(1)} %get-tuple-element.60), channel_id=1, source_target_pairs={{0,4},{2,6},{4,0},{6,2},{1,5},{3,7},{5,1},{7,3},{8,12},{10,14},{12... | collective-permute-start | bytes 208904 | tf_op jit(solution)/shard_map/ppermute | solution.py:489
  13.5 11.6 %collective-permute-start.7 = (s16[272,128]{1,0:T(8,128)(2,1)S(1)}, s16[272,128]{1,0:T(8,128)(2,1)S(1)}, u32[]{:S(2)}, u32[]{:S(2)}) collective-permute-start(s16[272,128]{1,0:T(8,128)(2,1)S(1)} %get-tuple-element.56), channel_id=1, source_target_pairs={{0,2},{2,0},{4,6},{6,4},{1,3},{3,1},{5,7},{7,5},{8,10},{10,8},{12,... | collective-permute-start | bytes 208904 | tf_op jit(solution)/shard_map/ppermute | solution.py:489
  15.5 11.4 %collective-permute-start.8 = (s16[272,128]{1,0:T(8,128)(2,1)S(1)}, s16[272,128]{1,0:T(8,128)(2,1)S(1)}, u32[]{:S(2)}, u32[]{:S(2)}) collective-permute-start(s16[272,128]{1,0:T(8,128)(2,1)S(1)} %get-tuple-element.57), channel_id=1, source_target_pairs={{0,4},{2,6},{4,0},{6,2},{1,5},{3,7},{5,1},{7,3},{8,12},{10,14},{12... | collective-permute-start | bytes 208904 | tf_op jit(solution)/shard_map/ppermute | solution.py:489
  17.0 9.9 %collective-permute-start.9 = (s16[272,128]{1,0:T(8,128)(2,1)S(1)}, s16[272,128]{1,0:T(8,128)(2,1)S(1)}, u32[]{:S(2)}, u32[]{:S(2)}) collective-permute-start(s16[272,128]{1,0:T(8,128)(2,1)S(1)} %get-tuple-element.58), channel_id=1, source_target_pairs={{0,6},{2,4},{4,2},{6,0},{1,7},{3,5},{5,3},{7,1},{8,14},{10,12},{12... | collective-permute-start | bytes 208904 | tf_op jit(solution)/shard_map/ppermute | solution.py:489
  18.3 11.4 %collective-permute-start.17 = (s16[272,128]{1,0:T(8,128)(2,1)S(1)}, s16[272,128]{1,0:T(8,128)(2,1)S(1)}, u32[]{:S(2)}, u32[]{:S(2)}) collective-permute-start(s16[272,128]{1,0:T(8,128)(2,1)S(1)} %level_states_0.1.refs_3_), channel_id=1, source_target_pairs={{0,8},{8,16},{16,24},{1,9},{9,17},{17,25},{2,10},{10,18},{18,26},{... | collective-permute-start | bytes 208904 | tf_op jit(solution)/shard_map/ppermute | solution.py:496
  21.7 9.9 %collective-permute-start.16 = (s16[272,128]{1,0:T(8,128)(2,1)S(1)}, s16[272,128]{1,0:T(8,128)(2,1)S(1)}, u32[]{:S(2)}, u32[]{:S(2)}) collective-permute-start(s16[272,128]{1,0:T(8,128)(2,1)S(1)} %level_states_0.1.refs_3_), channel_id=1, source_target_pairs={{0,24},{1,25},{2,26},{3,27},{4,28},{5,29},{6,30},{7,31}} | collective-permute-start | bytes 208904 | tf_op jit(solution)/shard_map/ppermute | solution.py:496
  25.1 6.6 %collective-permute-start.15 = (s16[272,128]{1,0:T(8,128)(2,1)S(1)}, s16[272,128]{1,0:T(8,128)(2,1)S(1)}, u32[]{:S(2)}, u32[]{:S(2)}) collective-permute-start(s16[272,128]{1,0:T(8,128)(2,1)S(1)} %level_states_0.1.refs_3_), channel_id=1, source_target_pairs={{0,16},{8,24},{1,17},{9,25},{2,18},{10,26},{3,19},{11,27},{4,20},{... | collective-permute-start | bytes 208904 | tf_op jit(solution)/shard_map/ppermute | solution.py:496
  27.1 7.6 %collective-permute-start.14 = (s16[272,128]{1,0:T(8,128)(2,1)S(1)}, s16[272,128]{1,0:T(8,128)(2,1)S(1)}, u32[]{:S(2)}, u32[]{:S(2)}) collective-permute-start(s16[272,128]{1,0:T(8,128)(2,1)S(1)} %level_states_1.1.refs_7_), channel_id=1, source_target_pairs={{0,24},{1,25},{2,26},{3,27},{4,28},{5,29},{6,30},{7,31}} | collective-permute-start | bytes 208904 | tf_op jit(solution)/shard_map/ppermute | solution.py:496
  28.4 6.3 %collective-permute-start.13 = (s16[272,128]{1,0:T(8,128)(2,1)S(1)}, s16[272,128]{1,0:T(8,128)(2,1)S(1)}, u32[]{:S(2)}, u32[]{:S(2)}) collective-permute-start(s16[272,128]{1,0:T(8,128)(2,1)S(1)} %level_states_1.1.refs_7_), channel_id=1, source_target_pairs={{0,16},{8,24},{1,17},{9,25},{2,18},{10,26},{3,19},{11,27},{4,20},{... | collective-permute-start | bytes 208904 | tf_op jit(solution)/shard_map/ppermute | solution.py:496
  29.7 5.0 %collective-permute-start.12 = (s16[272,128]{1,0:T(8,128)(2,1)S(1)}, s16[272,128]{1,0:T(8,128)(2,1)S(1)}, u32[]{:S(2)}, u32[]{:S(2)}) collective-permute-start(s16[272,128]{1,0:T(8,128)(2,1)S(1)} %level_states_1.1.refs_7_), channel_id=1, source_target_pairs={{0,8},{8,16},{16,24},{1,9},{9,17},{17,25},{2,10},{10,18},{18,26},{... | collective-permute-start | bytes 208904 | tf_op jit(solution)/shard_map/ppermute | solution.py:496
  31.9 5.3 %collective-permute-start.21 = (s16[272,128]{1,0:T(8,128)(2,1)S(1)}, s16[272,128]{1,0:T(8,128)(2,1)S(1)}, u32[]{:S(2)}, u32[]{:S(2)}) collective-permute-start(s16[272,128]{1,0:T(8,128)(2,1)S(1)} %get-tuple-element.65), channel_id=1, source_target_pairs={{0,6},{2,4},{4,2},{6,0},{1,7},{3,5},{5,3},{7,1},{8,14},{10,12},{12... | collective-permute-start | bytes 208904 | tf_op jit(solution)/shard_map/ppermute | solution.py:489
  33.7 4.6 %collective-permute-start.20 = (s16[272,128]{1,0:T(8,128)(2,1)S(1)}, s16[272,128]{1,0:T(8,128)(2,1)S(1)}, u32[]{:S(2)}, u32[]{:S(2)}) collective-permute-start(s16[272,128]{1,0:T(8,128)(2,1)S(1)} %get-tuple-element.61.refs_7_), channel_id=1, source_target_pairs={{0,2},{2,0},{4,6},{6,4},{1,3},{3,1},{5,7},{7,5},{8,10},{10,8},{12,... | collective-permute-start | bytes 208904 | tf_op jit(solution)/shard_map/ppermute | solution.py:489
  34.9 6.0 %collective-permute-start.19 = (s16[272,128]{1,0:T(8,128)(2,1)S(1)}, s16[272,128]{1,0:T(8,128)(2,1)S(1)}, u32[]{:S(2)}, u32[]{:S(2)}) collective-permute-start(s16[272,128]{1,0:T(8,128)(2,1)S(1)} %get-tuple-element.63), channel_id=1, source_target_pairs={{0,6},{2,4},{4,2},{6,0},{1,7},{3,5},{5,3},{7,1},{8,14},{10,12},{12... | collective-permute-start | bytes 208904 | tf_op jit(solution)/shard_map/ppermute | solution.py:489
  36.7 5.1 %collective-permute-start.18 = (s16[272,128]{1,0:T(8,128)(2,1)S(1)}, s16[272,128]{1,0:T(8,128)(2,1)S(1)}, u32[]{:S(2)}, u32[]{:S(2)}) collective-permute-start(s16[272,128]{1,0:T(8,128)(2,1)S(1)} %get-tuple-element.62.refs_10_), channel_id=1, source_target_pairs={{0,2},{2,0},{4,6},{6,4},{1,3},{3,1},{5,7},{7,5},{8,10},{10,8},{12,... | collective-permute-start | bytes 208904 | tf_op jit(solution)/shard_map/ppermute | solution.py:489
  39.7 16.6 %collective-permute-start.24 = (bf16[512,512]{1,0:T(8,128)(2,1)S(1)}, bf16[512,512]{1,0:T(8,128)(2,1)S(1)}, u32[]{:S(2)}, u32[]{:S(2)}) collective-permute-start(bf16[512,512]{1,0:T(8,128)(2,1)S(1)} %attend_0_1_3.1.refs_10_), channel_id=1, source_target_pairs={{0,2},{2,0},{1,3},{3,1},{4,6},{6,4},{5,7},{7,5},{8,10},{10,8},{9,1... | collective-permute-start | bytes 1572872 | tf_op jit(solution)/shard_map/ppermute | solution.py:489
  43.2 19.2 %collective-permute-start.22 = (bf16[512,512]{1,0:T(8,128)(2,1)S(1)}, bf16[512,512]{1,0:T(8,128)(2,1)S(1)}, u32[]{:S(2)}, u32[]{:S(2)}) collective-permute-start(bf16[512,512]{1,0:T(8,128)(2,1)S(1)} %attend_1_1_3.1.refs_14_.refs_10_), channel_id=1, source_target_pairs={{0,2},{2,0},{1,3},{3,1},{4,6},{6,4},{5,7},{7,5},{8,10},{10,8},{9,1... | collective-permute-start | bytes 1572872 | tf_op jit(solution)/shard_map/ppermute | solution.py:489
  44.8 10.5 %collective-permute-start.25 = (f32[2,2,128,128]{3,2,1,0:T(8,128)S(1)}, f32[2,2,128,128]{3,2,1,0:T(8,128)S(1)}, u32[]{:S(2)}, u32[]{:S(2)}) collective-permute-start(f32[2,2,128,128]{3,2,1,0:T(8,128)S(1)} %get-tuple-element.69), channel_id=1, source_target_pairs={{0,4},{4,0},{1,5},{5,1},{2,6},{6,2},{3,7},{7,3},{8,12},{12,8},{9,1... | collective-permute-start | bytes 786440 | tf_op jit(solution)/shard_map/ppermute | solution.py:489
  46.2 6.5 %collective-permute-start.23 = (s16[528,128]{1,0:T(8,128)(2,1)S(1)}, s16[528,128]{1,0:T(8,128)(2,1)S(1)}, u32[]{:S(2)}, u32[]{:S(2)}) collective-permute-start(s16[528,128]{1,0:T(8,128)(2,1)S(1)} %get-tuple-element.67), channel_id=1, source_target_pairs={{0,4},{2,6},{4,0},{6,2},{1,5},{3,7},{5,1},{7,3},{8,12},{10,14},{12... | collective-permute-start | bytes 405512 | tf_op jit(solution)/shard_map/ppermute | solution.py:489

commit v17 on v16

--- a/solution.py
+++ b/solution.py
@@ -12,7 +12,7 @@
 SCORE_SCALE = HD ** (-0.5)
 CORES = 2
 VMEM_BYTES = 24 * 1024 * 1024
-DECODE_VMEM_BYTES = 46 * 1024 * 1024
+DECODE_VMEM_BYTES = 50 * 1024 * 1024
 PAD = 16
 TOP = 32767.0
 
@@ -78,53 +78,61 @@
                 yield side, half, slice(y * width, (y + 1) * width), at
 
 
-def decode(plan, spikes, keys, values):
-    rows, model = spikes.shape
-    step = min(rows, 32)
+def decode(plan, spikes, keys, values, half):
+    rows, _ = spikes.shape
+    step = min(rows, 64)
     chunks = rows // step
-    n_out = 3 * CORES * plan.halves
+    width = plan.half_width
+    groups = plan.n_y * CORES
 
     def kernel(*refs):
         core = lax.axis_index("core")
-        sources, *outs, b0, b1, b2, sems = refs[:3], *refs[3:]
-        buffers = (b0, b1, b2)
-
-        def fetch(chunk, index):
+        sources, outs, buffers, sems = refs[:3], refs[3:9], refs[9:12], refs[12]
+
+        def fetch(chunk, index, group):
             at = pl.ds(chunk * step, step)
+            columns = pl.ds((group * plan.halves + half) * width, width)
             return pltpu.make_async_copy(
-                sources[index].at[at], buffers[index].at[at], sems.at[chunk, index]
+                sources[index].at[at, columns],
+                buffers[index].at[at, pl.ds(group * width, width)],
+                sems.at[chunk, index, group],
             )
 
+        every = [(index, group) for index in range(3) for group in range(groups)]
         for chunk in range(chunks):
-            for index in range(3):
-                fetch(chunk, index).start()
+            for index, group in every:
+                fetch(chunk, index, group).start()
 
         @pl.loop(0, chunks)
         def _(chunk):
-            for index in range(3):
-                fetch(chunk, index).wait()
+            for index, group in every:
+                fetch(chunk, index, group).wait()
             at = pl.ds(pl.multiple_of(chunk * step, step), step)
-            for side, half, mine, columns in sides(plan, core):
-                spikes = buffers[0][at, columns].astype(jnp.float32).astype(jnp.bfloat16)
-                value, key, query = counts_of(spikes)
-                spiked = (buffers[1][at, columns] * key, buffers[2][at, columns] * value, query)
-                for index, array in enumerate(spiked):
-                    outs[(index * CORES + side) * plan.halves + half][at, mine] = array
+            for y in range(plan.n_y):
+                mine = slice(y * width, (y + 1) * width)
+                for side in range(CORES):
+                    of = core if side == 0 else 1 - core
+                    columns = pl.ds(pl.multiple_of((y * CORES + of) * width, width), width)
+                    codes = buffers[0][at, columns].astype(jnp.float32).astype(jnp.bfloat16)
+                    value, key, query = counts_of(codes)
+                    outs[side][at, mine] = buffers[1][at, columns] * key
+                    outs[2 + side][at, mine] = buffers[2][at, columns] * value
+                    outs[4 + side][at, mine] = query
 
     return pl.pallas_call(
         kernel,
-        out_shape=[jax.ShapeDtypeStruct((rows, plan.n_y * plan.half_width), jnp.bfloat16)] * n_out,
+        out_shape=[jax.ShapeDtypeStruct((rows, plan.n_y * width), jnp.bfloat16)] * 6,
         in_specs=[HBM] * 3,
-        out_specs=[VMEM] * n_out,
+        out_specs=[VMEM] * 6,
         scratch_shapes=[
-            pltpu.VMEM((rows, model), jnp.int32),
-            pltpu.VMEM((rows, model), jnp.bfloat16),
-            pltpu.VMEM((rows, model), jnp.bfloat16),
-            pltpu.SemaphoreType.DMA((chunks, 3)),
+            pltpu.VMEM((rows, groups * width), jnp.int32),
+            pltpu.VMEM((rows, groups * width), jnp.bfloat16),
+            pltpu.VMEM((rows, groups * width), jnp.bfloat16),
+            pltpu.SemaphoreType.DMA((chunks, 3, groups)),
         ],
         compiler_params=params(DECODE_VMEM_BYTES),
-        cost_estimate=cost(rows * model * 4, rows * model * 14),
-        name="decode",
+        cost_estimate=cost(rows * groups * width * 4, rows * groups * width * 14),
+        name=f"decode_{half}",
     )(spikes, keys, values)
 
 
@@ -496,8 +504,8 @@
         return lax.ppermute(array, "outer", pairs)
 
     gain = gain.reshape(1, plan.width)
-    arrays = decode(plan, spikes, keys, values)
-    parts = [arrays[k : k + plan.halves] for k in range(0, len(arrays), plan.halves)]
+    arrays = [decode(plan, spikes, keys, values, half) for half in halves]
+    parts = [list(of_halves) for of_halves in zip(*arrays)]
 
     def with_siblings(mine, theirs):
         return [(a, swap(b, "core", 1, CORES)) for a, b in zip(mine, theirs)]

time: 63.5 us -> 64.6 us (1.017)
  Pallas kernels: 15.1 us -> 17 us
    pallas_call x1 -> x2, Pallas kernels: 3.88 us -> 5.73 us  [decode(): pl.pallas_call(kernel, out_shape=[jax.ShapeDtypeStruct((rows, plan.n_y *...]
  transfers between devices with their start and end apart: 26 -> 26, of which waited for: 6 -> 4; matrix products, arithmetic and copies ran while one was open for 0% -> 0% of each run, Pallas kernels for 17% -> 21%
where the time goes in v17:
time: 64.6 us; the launch traced here: 64.3 us
  starting transfers between devices  33.6 us (52%)
  Pallas kernels  17 us (26%)
  waiting for transfers between devices  12.9 us (20%)
  between operations  0.84 us (1%)
    ppermute x20, starting transfers between devices, swap(): return lax.ppermute(array, axes, [(i, i ^ offset) for i in range(size)])  20.4 us
    ppermute x6, starting transfers between devices, to_later(): return lax.ppermute(array, 'outer', pairs)  13.2 us
    ppermute x20, waiting for transfers between devices, swap(): return lax.ppermute(array, axes, [(i, i ^ offset) for i in range(size)])  12.9 us
    pallas_call x2, Pallas kernels, decode(): pl.pallas_call(kernel, out_shape=[jax.ShapeDtypeStruct((rows, plan.n_y *...  5.73 us
    pallas_call x4, Pallas kernels, attend(): pl.pallas_call(at_place(kernel), out_shape=jax.ShapeDtypeStruct((CORES *...  5.3 us
    pallas_call x2, Pallas kernels, assemble(): pl.pallas_call(at_place(kernel), out_shape=jax.ShapeDtypeStruct((plan.n_y...  1.99 us
    pallas_call x2, Pallas kernels, chunk_states(): pl.pallas_call(at_place(kernel), out_shape=[states_shape(plan.each), stat...  1.64 us
  transfers between devices with their start and end apart: 26, of which 4 were waited for; matrix products, arithmetic and copies ran while one was open for 0% of the time, Pallas kernels for 21%

profile of v17, /device:TPU:0, one launch (start us, length us, event | category | flops | bytes accessed | tf_op | source)
XLA Modules:
  0.0 64.3 jit_solution(10768466403582069785)
XLA Ops:
  0.6 2.8 %decode_0.1 = (bf16[256,1024]{1,0:T(8,128)(2,1)S(1)}, bf16[256,1024]{1,0:T(8,128)(2,1)S(1)}, bf16[256,1024]{1,0:T(8,128)(2,1)S(1)}, bf16[256,1024]{1,0:T(8,128)(...) custom-call(s32[256,4096]{1,0:T(8,128)} %refs_0_.4, bf16[256,4096]{1,0:T(8,128)(2,1)} %refs_1_.3, ...), custom_call_target="tpu_custom_call" | custom-call | flops 2097152 | bytes 7340032 | tf_op jit(solution)/shard_map/decode_0/pallas_call | solution.py:122
  3.4 0.5 collective-permute-start.3
  4.0 0.1 collective-permute-start.4
  4.1 2.9 %decode_1.1 = (bf16[256,1024]{1,0:T(8,128)(2,1)S(1)}, bf16[256,1024]{1,0:T(8,128)(2,1)S(1)}, bf16[256,1024]{1,0:T(8,128)(2,1)S(1)}, bf16[256,1024]{1,0:T(8,128)(...) custom-call(s32[256,4096]{1,0:T(8,128)} %refs_0_.4, bf16[256,4096]{1,0:T(8,128)(2,1)} %refs_1_.3, ...), custom_call_target="tpu_custom_call" | custom-call | flops 2097152 | bytes 7340032 | tf_op jit(solution)/shard_map/decode_1/pallas_call | solution.py:122
  7.0 0.5 collective-permute-start.1
  7.5 0.1 collective-permute-start.2
  7.6 0.3 spike_queries.1
  7.9 0.5 collective-permute-start
  8.4 0.0 collective-permute-done.3.refs_1_.refs_3_
  8.4 0.1 collective-permute-start.5
  8.5 0.0 collective-permute-done.4.refs_3_.refs_5_
  8.5 0.8 %chunk_states_0.1 = (f32[2,128,128]{2,1,0:T(8,128)S(1)}, f32[4,2,128,128]{3,2,1,0:T(8,128)S(1)}, s16[288,128]{1,0:T(8,128)(2,1)S(1)}, s16[272,128]{1,0:T(8,128)(2,1)S(1)}, s16[272,128]{1,0:T(8,128)(2,1)S(1)}) custom-call(bf16[256,1024]{1,0:T(8,128)(2,1)S(1)} %get-tuple-element.46.refs_0_.refs_2_, ...), custom_call_target="tpu_custom_call" | custom-call | flops 134217728 | bytes 2883584 | tf_op jit(solution)/shard_map/chunk_states_0/pallas_call | solution.py:259
  9.3 3.0 %collective-permute-start.6 = (s16[288,128]{1,0:T(8,128)(2,1)S(1)}, s16[288,128]{1,0:T(8,128)(2,1)S(1)}, u32[]{:S(2)}, u32[]{:S(2)}) collective-permute-start(s16[288,128]{1,0:T(8,128)(2,1)S(1)} %get-tuple-element.54), channel_id=1, source_target_pairs={{0,2},{2,0},{4,6},{6,4},{1,3},{3,1},{5,7},{7,5},{8,10},{10,8},{12,... | collective-permute-start | bytes 221192 | tf_op jit(solution)/shard_map/ppermute | solution.py:497
  12.3 0.0 collective-permute-done.1.refs_1_.refs_3_
  12.3 1.4 %collective-permute-start.10 = (s16[272,128]{1,0:T(8,128)(2,1)S(1)}, s16[272,128]{1,0:T(8,128)(2,1)S(1)}, u32[]{:S(2)}, u32[]{:S(2)}) collective-permute-start(s16[272,128]{1,0:T(8,128)(2,1)S(1)} %get-tuple-element.59), channel_id=1, source_target_pairs={{0,6},{2,4},{4,2},{6,0},{1,7},{3,5},{5,3},{7,1},{8,14},{10,12},{12... | collective-permute-start | bytes 208904 | tf_op jit(solution)/shard_map/ppermute | solution.py:497
  13.7 0.0 collective-permute-done.2.refs_3_.refs_5_
  13.7 0.1 collective-permute-start.11
  13.8 0.0 collective-permute-done.refs_6_.refs_5_.refs_1_
  13.8 0.0 collective-permute-done.5.refs_5_.refs_4_.refs_1_
  13.8 0.8 %chunk_states_1.1 = (f32[2,128,128]{2,1,0:T(8,128)S(1)}, f32[4,2,128,128]{3,2,1,0:T(8,128)S(1)}, s16[272,128]{1,0:T(8,128)(2,1)S(1)}, s16[272,128]{1,0:T(8,128)(2,1)S(1)}, s16[272,128]{1,0:T(8,128)(2,1)S(1)}) custom-call(bf16[256,1024]{1,0:T(8,128)(2,1)S(1)} %get-tuple-element.42.refs_0_.refs_2_, ...), custom_call_target="tpu_custom_call" | custom-call | flops 134217728 | bytes 2883584 | tf_op jit(solution)/shard_map/chunk_states_1/pallas_call | solution.py:259
  14.7 2.0 %collective-permute-start.7 = (s16[272,128]{1,0:T(8,128)(2,1)S(1)}, s16[272,128]{1,0:T(8,128)(2,1)S(1)}, u32[]{:S(2)}, u32[]{:S(2)}) collective-permute-start(s16[272,128]{1,0:T(8,128)(2,1)S(1)} %get-tuple-element.56), channel_id=1, source_target_pairs={{0,2},{2,0},{4,6},{6,4},{1,3},{3,1},{5,7},{7,5},{8,10},{10,8},{12,... | collective-permute-start | bytes 208904 | tf_op jit(solution)/shard_map/ppermute | solution.py:497
  16.7 1.5 %collective-permute-start.8 = (s16[272,128]{1,0:T(8,128)(2,1)S(1)}, s16[272,128]{1,0:T(8,128)(2,1)S(1)}, u32[]{:S(2)}, u32[]{:S(2)}) collective-permute-start(s16[272,128]{1,0:T(8,128)(2,1)S(1)} %get-tuple-element.57), channel_id=1, source_target_pairs={{0,4},{2,6},{4,0},{6,2},{1,5},{3,7},{5,1},{7,3},{8,12},{10,14},{12... | collective-permute-start | bytes 208904 | tf_op jit(solution)/shard_map/ppermute | solution.py:497
  18.1 0.0 collective-permute-done.10.refs_0_.refs_3_
  18.2 1.1 %collective-permute-start.9 = (s16[272,128]{1,0:T(8,128)(2,1)S(1)}, s16[272,128]{1,0:T(8,128)(2,1)S(1)}, u32[]{:S(2)}, u32[]{:S(2)}) collective-permute-start(s16[272,128]{1,0:T(8,128)(2,1)S(1)} %get-tuple-element.58), channel_id=1, source_target_pairs={{0,6},{2,4},{4,2},{6,0},{1,7},{3,5},{5,3},{7,1},{8,14},{10,12},{12... | collective-permute-start | bytes 208904 | tf_op jit(solution)/shard_map/ppermute | solution.py:497
  19.2 0.0 collective-permute-done.11.refs_1_.refs_2_
  19.2 0.0 collective-permute-done.6.refs_2_.refs_1_.refs_7_
  19.2 0.1 level_states_0.1.refs_3_
  19.3 3.5 %collective-permute-start.17 = (s16[272,128]{1,0:T(8,128)(2,1)S(1)}, s16[272,128]{1,0:T(8,128)(2,1)S(1)}, u32[]{:S(2)}, u32[]{:S(2)}) collective-permute-start(s16[272,128]{1,0:T(8,128)(2,1)S(1)} %level_states_0.1.refs_3_), channel_id=1, source_target_pairs={{0,8},{8,16},{16,24},{1,9},{9,17},{17,25},{2,10},{10,18},{18,26},{... | collective-permute-start | bytes 208904 | tf_op jit(solution)/shard_map/ppermute | solution.py:504
  22.8 3.3 %collective-permute-start.16 = (s16[272,128]{1,0:T(8,128)(2,1)S(1)}, s16[272,128]{1,0:T(8,128)(2,1)S(1)}, u32[]{:S(2)}, u32[]{:S(2)}) collective-permute-start(s16[272,128]{1,0:T(8,128)(2,1)S(1)} %level_states_0.1.refs_3_), channel_id=1, source_target_pairs={{0,24},{1,25},{2,26},{3,27},{4,28},{5,29},{6,30},{7,31}} | collective-permute-start | bytes 208904 | tf_op jit(solution)/shard_map/ppermute | solution.py:504
  26.2 0.0 collective-permute-done.7.refs_2_.refs_1_.refs_8_
  26.2 1.8 %collective-permute-start.15 = (s16[272,128]{1,0:T(8,128)(2,1)S(1)}, s16[272,128]{1,0:T(8,128)(2,1)S(1)}, u32[]{:S(2)}, u32[]{:S(2)}) collective-permute-start(s16[272,128]{1,0:T(8,128)(2,1)S(1)} %level_states_0.1.refs_3_), channel_id=1, source_target_pairs={{0,16},{8,24},{1,17},{9,25},{2,18},{10,26},{3,19},{11,27},{4,20},{... | collective-permute-start | bytes 208904 | tf_op jit(solution)/shard_map/ppermute | solution.py:504
  28.0 0.0 collective-permute-done.8.refs_1_.refs_2_.refs_9_
  28.0 0.0 collective-permute-done.9.refs_0_.refs_3_.refs_10_
  28.0 0.1 level_states_1.1.refs_7_
  28.2 1.3 %collective-permute-start.14 = (s16[272,128]{1,0:T(8,128)(2,1)S(1)}, s16[272,128]{1,0:T(8,128)(2,1)S(1)}, u32[]{:S(2)}, u32[]{:S(2)}) collective-permute-start(s16[272,128]{1,0:T(8,128)(2,1)S(1)} %level_states_1.1.refs_7_), channel_id=1, source_target_pairs={{0,24},{1,25},{2,26},{3,27},{4,28},{5,29},{6,30},{7,31}} | collective-permute-start | bytes 208904 | tf_op jit(solution)/shard_map/ppermute | solution.py:504
  29.5 1.3 %collective-permute-start.13 = (s16[272,128]{1,0:T(8,128)(2,1)S(1)}, s16[272,128]{1,0:T(8,128)(2,1)S(1)}, u32[]{:S(2)}, u32[]{:S(2)}) collective-permute-start(s16[272,128]{1,0:T(8,128)(2,1)S(1)} %level_states_1.1.refs_7_), channel_id=1, source_target_pairs={{0,16},{8,24},{1,17},{9,25},{2,18},{10,26},{3,19},{11,27},{4,20},{... | collective-permute-start | bytes 208904 | tf_op jit(solution)/shard_map/ppermute | solution.py:504
  30.8 0.0 collective-permute-done.17.refs_6_
  30.8 2.0 %collective-permute-start.12 = (s16[272,128]{1,0:T(8,128)(2,1)S(1)}, s16[272,128]{1,0:T(8,128)(2,1)S(1)}, u32[]{:S(2)}, u32[]{:S(2)}) collective-permute-start(s16[272,128]{1,0:T(8,128)(2,1)S(1)} %level_states_1.1.refs_7_), channel_id=1, source_target_pairs={{0,8},{8,16},{16,24},{1,9},{9,17},{17,25},{2,10},{10,18},{18,26},{... | collective-permute-start | bytes 208904 | tf_op jit(solution)/shard_map/ppermute | solution.py:504
  32.8 0.0 collective-permute-done.16.refs_5_
  32.8 0.2 carries_0.1
  33.0 1.8 %collective-permute-start.21 = (s16[272,128]{1,0:T(8,128)(2,1)S(1)}, s16[272,128]{1,0:T(8,128)(2,1)S(1)}, u32[]{:S(2)}, u32[]{:S(2)}) collective-permute-start(s16[272,128]{1,0:T(8,128)(2,1)S(1)} %get-tuple-element.65), channel_id=1, source_target_pairs={{0,6},{2,4},{4,2},{6,0},{1,7},{3,5},{5,3},{7,1},{8,14},{10,12},{12... | collective-permute-start | bytes 208904 | tf_op jit(solution)/shard_map/ppermute | solution.py:497
  34.8 0.9 %collective-permute-start.20 = (s16[272,128]{1,0:T(8,128)(2,1)S(1)}, s16[272,128]{1,0:T(8,128)(2,1)S(1)}, u32[]{:S(2)}, u32[]{:S(2)}) collective-permute-start(s16[272,128]{1,0:T(8,128)(2,1)S(1)} %get-tuple-element.61.refs_7_), channel_id=1, source_target_pairs={{0,2},{2,0},{4,6},{6,4},{1,3},{3,1},{5,7},{7,5},{8,10},{10,8},{12,... | collective-permute-start | bytes 208904 | tf_op jit(solution)/shard_map/ppermute | solution.py:497
  35.8 0.0 collective-permute-done.12.refs_4_.refs_11_
  35.8 0.2 carries_1.1
  36.0 1.8 %collective-permute-start.19 = (s16[272,128]{1,0:T(8,128)(2,1)S(1)}, s16[272,128]{1,0:T(8,128)(2,1)S(1)}, u32[]{:S(2)}, u32[]{:S(2)}) collective-permute-start(s16[272,128]{1,0:T(8,128)(2,1)S(1)} %get-tuple-element.63), channel_id=1, source_target_pairs={{0,6},{2,4},{4,2},{6,0},{1,7},{3,5},{5,3},{7,1},{8,14},{10,12},{12... | collective-permute-start | bytes 208904 | tf_op jit(solution)/shard_map/ppermute | solution.py:497
  37.8 0.5 collective-permute-start.18
  38.3 0.0 collective-permute-done.21.refs_9_
  38.3 1.1 %collective-permute-done.20.refs_8_ = s16[272,128]{1,0:T(8,128)(2,1)S(1)} collective-permute-done((s16[272,128]{1,0:T(8,128)(2,1)S(1)}, s16[272,128]{1,0:T(8,128)(2,1)S(1)}, u32[]{:S(2)}, u32[]{:S(2)}) %collective-permute-start.20) | collective-permute-done | bytes 69664 | tf_op jit(solution)/shard_map/ppermute | solution.py:497
  39.4 1.3 %attend_0_1_3.1.refs_10_ = bf16[512,512]{1,0:T(8,128)(2,1)S(1)} custom-call(bf16[256,1024]{1,0:T(8,128)(2,1)S(1)} %get-tuple-element.50.refs_5_.refs_0_, bf16[256,1024]{1,0:T(8,128)(2,1)S(1)} %collective-permute-done.5.refs_5_.refs_4_.refs_1_, bf16[256,1024]{1,0:T(8,128)(2,1)S(1)} %get-tuple-element.46.refs_0_.refs_2_, ...), custom_call_target="tpu_custom_call" | custom-call | flops 402653184 | bytes 2097152 | tf_op jit(solution)/shard_map/attend_0_1_3/pallas_call | solution.py:423
  40.7 1.3 %collective-permute-start.24 = (bf16[512,512]{1,0:T(8,128)(2,1)S(1)}, bf16[512,512]{1,0:T(8,128)(2,1)S(1)}, u32[]{:S(2)}, u32[]{:S(2)}) collective-permute-start(bf16[512,512]{1,0:T(8,128)(2,1)S(1)} %attend_0_1_3.1.refs_10_), channel_id=1, source_target_pairs={{0,2},{2,0},{1,3},{3,1},{4,6},{6,4},{5,7},{7,5},{8,10},{10,8},{9,1... | collective-permute-start | bytes 1572872 | tf_op jit(solution)/shard_map/ppermute | solution.py:497
  42.0 0.0 collective-permute-done.19.refs_9_
  42.0 1.0 %collective-permute-done.18.refs_8_ = s16[272,128]{1,0:T(8,128)(2,1)S(1)} collective-permute-done((s16[272,128]{1,0:T(8,128)(2,1)S(1)}, s16[272,128]{1,0:T(8,128)(2,1)S(1)}, u32[]{:S(2)}, u32[]{:S(2)}) %collective-permute-start.18) | collective-permute-done | bytes 69664 | tf_op jit(solution)/shard_map/ppermute | solution.py:497
  43.0 1.3 %attend_1_1_3.1.refs_14_.refs_10_ = bf16[512,512]{1,0:T(8,128)(2,1)S(1)} custom-call(bf16[256,1024]{1,0:T(8,128)(2,1)S(1)} %get-tuple-element.40.refs_0_, bf16[256,1024]{1,0:T(8,128)(2,1)S(1)} %collective-permute-done.refs_6_.refs_5_.refs_1_, bf16[256,1024]{1,0:T(8,128)(2,1)S(1)} %get-tuple-element.42.refs_0_.refs_2_, ...), custom_call_target="tpu_custom_call" | custom-call | flops 402653184 | bytes 2097152 | tf_op jit(solution)/shard_map/attend_1_1_3/pallas_call | solution.py:423
  44.3 1.1 %collective-permute-start.22 = (bf16[512,512]{1,0:T(8,128)(2,1)S(1)}, bf16[512,512]{1,0:T(8,128)(2,1)S(1)}, u32[]{:S(2)}, u32[]{:S(2)}) collective-permute-start(bf16[512,512]{1,0:T(8,128)(2,1)S(1)} %attend_1_1_3.1.refs_14_.refs_10_), channel_id=1, source_target_pairs={{0,2},{2,0},{1,3},{3,1},{4,6},{6,4},{5,7},{7,5},{8,10},{10,8},{9,1... | collective-permute-start | bytes 1572872 | tf_op jit(solution)/shard_map/ppermute | solution.py:497
  45.4 0.6 own_carries.1
  45.9 1.4 %collective-permute-start.25 = (f32[2,2,128,128]{3,2,1,0:T(8,128)S(1)}, f32[2,2,128,128]{3,2,1,0:T(8,128)S(1)}, u32[]{:S(2)}, u32[]{:S(2)}) collective-permute-start(f32[2,2,128,128]{3,2,1,0:T(8,128)S(1)} %get-tuple-element.69), channel_id=1, source_target_pairs={{0,4},{4,0},{1,5},{5,1},{2,6},{6,2},{3,7},{7,3},{8,12},{12,8},{9,1... | collective-permute-start | bytes 786440 | tf_op jit(solution)/shard_map/ppermute | solution.py:497
  47.3 0.7 %collective-permute-start.23 = (s16[528,128]{1,0:T(8,128)(2,1)S(1)}, s16[528,128]{1,0:T(8,128)(2,1)S(1)}, u32[]{:S(2)}, u32[]{:S(2)}) collective-permute-start(s16[528,128]{1,0:T(8,128)(2,1)S(1)} %get-tuple-element.67), channel_id=1, source_target_pairs={{0,4},{2,6},{4,0},{6,2},{1,5},{3,7},{5,1},{7,3},{8,12},{10,14},{12... | collective-permute-start | bytes 405512 | tf_op jit(solution)/shard_map/ppermute | solution.py:497
  48.0 5.8 %collective-permute-done.23.refs_9_ = s16[528,128]{1,0:T(8,128)(2,1)S(1)} collective-permute-done((s16[528,128]{1,0:T(8,128)(2,1)S(1)}, s16[528,128]{1,0:T(8,128)(2,1)S(1)}, u32[]{:S(2)}, u32[]{:S(2)}) %collective-permute-start.23) | collective-permute-done | bytes 135200 | tf_op jit(solution)/shard_map/ppermute | solution.py:497
  53.8 1.3 %attend_0_0_2.1.refs_10_.refs_0_ = bf16[512,512]{1,0:T(8,128)(2,1)S(1)} custom-call(bf16[256,1024]{1,0:T(8,128)(2,1)S(1)} %get-tuple-element.50.refs_5_.refs_0_, bf16[256,1024]{1,0:T(8,128)(2,1)S(1)} %collective-permute-done.5.refs_5_.refs_4_.refs_1_, bf16[256,1024]{1,0:T(8,128)(2,1)S(1)} %get-tuple-element.46.refs_0_.refs_2_, ...), custom_call_target="tpu_custom_call" | custom-call | flops 402653184 | bytes 2097152 | tf_op jit(solution)/shard_map/attend_0_0_2/pallas_call | solution.py:423
  55.1 1.3 %attend_1_0_2.1.refs_1_ = bf16[512,512]{1,0:T(8,128)(2,1)S(1)} custom-call(bf16[256,1024]{1,0:T(8,128)(2,1)S(1)} %get-tuple-element.40.refs_0_, bf16[256,1024]{1,0:T(8,128)(2,1)S(1)} %collective-permute-done.refs_6_.refs_5_.refs_1_, bf16[256,1024]{1,0:T(8,128)(2,1)S(1)} %get-tuple-element.42.refs_0_.refs_2_, ...), custom_call_target="tpu_custom_call" | custom-call | flops 402653184 | bytes 2097152 | tf_op jit(solution)/shard_map/attend_1_0_2/pallas_call | solution.py:423
  56.5 0.8 %assemble_cache.1 = f32[1,8,128,128]{3,2,1,0:T(8,128)} custom-call(f32[2,2,128,128]{3,2,1,0:T(8,128)S(1)} %get-tuple-element.68.refs_0_, f32[2,2,128,128]{3,2,1,0:T(8,128)S(1)} %collective-permute-done.25.refs_1_), custom_call_target="tpu_custom_call" | custom-call | tf_op jit(solution)/shard_map/assemble_cache/pallas_call | solution.py:483
  57.3 1.2 %assemble.1.refs_1_ = bf16[1024,1024]{1,0:T(8,128)(2,1)} custom-call(bf16[512,512]{1,0:T(8,128)(2,1)S(1)} %attend_0_0_2.1.refs_10_.refs_0_, bf16[512,512]{1,0:T(8,128)(2,1)S(1)} %attend_1_0_2.1.refs_1_, bf16[512,512]{1,0:T(8,128)(2,1)S(1)} %collective-permute-done.24.refs_2_), custom_call_target="tpu_custom_call" | custom-call | tf_op jit(solution)/shard_map/assemble/pallas_call | solution.py:462
  58.5 5.0 %collective-permute-done.22.refs_0_ = bf16[512,512]{1,0:T(8,128)(2,1)S(1)} collective-permute-done((bf16[512,512]{1,0:T(8,128)(2,1)S(1)}, bf16[512,512]{1,0:T(8,128)(2,1)S(1)}, u32[]{:S(2)}, u32[]{:S(2)}) %collective-permute-start.22) | collective-permute-done | bytes 524320 | tf_op jit(solution)/shard_map/ppermute | solution.py:497
  63.5 0.8 %finish.1 = bf16[1024,1024]{1,0:T(8,128)(2,1)} custom-call(bf16[512,512]{1,0:T(8,128)(2,1)S(1)} %collective-permute-done.22.refs_0_, bf16[1024,1024]{1,0:T(8,128)(2,1)} %assemble.1.refs_1_), custom_call_target="tpu_custom_call", output_to_operand_aliasing={{}: (1, {})} | custom-call | tf_op jit(solution)/shard_map/finish/pallas_call | solution.py:462
  (9 shorter events, 0.0 us)
Async XLA Ops:
  3.4 4.9 %collective-permute-start.3 = (bf16[256,1024]{1,0:T(8,128)(2,1)S(1)}, bf16[256,1024]{1,0:T(8,128)(2,1)S(1)}, u32[]{:S(2)}, u32[]{:S(2)}) collective-permute-start(bf16[256,1024]{1,0:T(8,128)(2,1)S(1)} %get-tuple-element.47), channel_id=1, source_target_pairs={{0,1},{1,0},{2,3},{3,2},{4,5},{5,4},{6,7},{7,6},{8,9},{9,8},{10,11... | collective-permute-start | bytes 1572872 | tf_op jit(solution)/shard_map/ppermute | solution.py:497
  4.0 3.6 %copy-start = (bf16[256,4096]{1,0:T(8,128)(2,1)S(1)}, bf16[256,4096]{1,0:T(8,128)(2,1)}, u32[]{:S(2)}) copy-start(bf16[256,4096]{1,0:T(8,128)(2,1)} %refs_0_.5) | copy-start | bytes 6291460
  4.0 4.5 %collective-permute-start.4 = (bf16[256,1024]{1,0:T(8,128)(2,1)S(1)}, bf16[256,1024]{1,0:T(8,128)(2,1)S(1)}, u32[]{:S(2)}, u32[]{:S(2)}) collective-permute-start(bf16[256,1024]{1,0:T(8,128)(2,1)S(1)} %get-tuple-element.49), channel_id=1, source_target_pairs={{0,1},{1,0},{2,3},{3,2},{4,5},{5,4},{6,7},{7,6},{8,9},{9,8},{10,11... | collective-permute-start | bytes 1572872 | tf_op jit(solution)/shard_map/ppermute | solution.py:497
  7.0 5.3 %collective-permute-start.1 = (bf16[256,1024]{1,0:T(8,128)(2,1)S(1)}, bf16[256,1024]{1,0:T(8,128)(2,1)S(1)}, u32[]{:S(2)}, u32[]{:S(2)}) collective-permute-start(bf16[256,1024]{1,0:T(8,128)(2,1)S(1)} %get-tuple-element.43), channel_id=1, source_target_pairs={{0,1},{1,0},{2,3},{3,2},{4,5},{5,4},{6,7},{7,6},{8,9},{9,8},{10,11... | collective-permute-start | bytes 1572872 | tf_op jit(solution)/shard_map/ppermute | solution.py:497
  7.5 6.2 %collective-permute-start.2 = (bf16[256,1024]{1,0:T(8,128)(2,1)S(1)}, bf16[256,1024]{1,0:T(8,128)(2,1)S(1)}, u32[]{:S(2)}, u32[]{:S(2)}) collective-permute-start(bf16[256,1024]{1,0:T(8,128)(2,1)S(1)} %get-tuple-element.45), channel_id=1, source_target_pairs={{0,1},{1,0},{2,3},{3,2},{4,5},{5,4},{6,7},{7,6},{8,9},{9,8},{10,11... | collective-permute-start | bytes 1572872 | tf_op jit(solution)/shard_map/ppermute | solution.py:497
  7.6 0.9 %copy-start.1 = (f32[1024]{0:T(1024)S(1)}, f32[1024]{0:T(1024)}, u32[]{:S(2)}) copy-start(f32[1024]{0:T(1024)} %param.9) | copy-start | bytes 12292
  7.9 5.9 %collective-permute-start = (bf16[256,1024]{1,0:T(8,128)(2,1)S(1)}, bf16[256,1024]{1,0:T(8,128)(2,1)S(1)}, u32[]{:S(2)}, u32[]{:S(2)}) collective-permute-start(bf16[256,1024]{1,0:T(8,128)(2,1)S(1)} %get-tuple-element.41), channel_id=1, source_target_pairs={{0,1},{1,0},{2,3},{3,2},{4,5},{5,4},{6,7},{7,6},{8,9},{9,8},{10,11... | collective-permute-start | bytes 1572872 | tf_op jit(solution)/shard_map/ppermute | solution.py:497
  8.4 5.5 %collective-permute-start.5 = (bf16[256,1024]{1,0:T(8,128)(2,1)S(1)}, bf16[256,1024]{1,0:T(8,128)(2,1)S(1)}, u32[]{:S(2)}, u32[]{:S(2)}) collective-permute-start(bf16[256,1024]{1,0:T(8,128)(2,1)S(1)} %get-tuple-element.52), channel_id=1, source_target_pairs={{0,1},{1,0},{2,3},{3,2},{4,5},{5,4},{6,7},{7,6},{8,9},{9,8},{10,11... | collective-permute-start | bytes 1572872 | tf_op jit(solution)/shard_map/ppermute | solution.py:497
  9.3 10.0 %collective-permute-start.6 = (s16[288,128]{1,0:T(8,128)(2,1)S(1)}, s16[288,128]{1,0:T(8,128)(2,1)S(1)}, u32[]{:S(2)}, u32[]{:S(2)}) collective-permute-start(s16[288,128]{1,0:T(8,128)(2,1)S(1)} %get-tuple-element.54), channel_id=1, source_target_pairs={{0,2},{2,0},{4,6},{6,4},{1,3},{3,1},{5,7},{7,5},{8,10},{10,8},{12,... | collective-permute-start | bytes 221192 | tf_op jit(solution)/shard_map/ppermute | solution.py:497
  12.3 5.9 %collective-permute-start.10 = (s16[272,128]{1,0:T(8,128)(2,1)S(1)}, s16[272,128]{1,0:T(8,128)(2,1)S(1)}, u32[]{:S(2)}, u32[]{:S(2)}) collective-permute-start(s16[272,128]{1,0:T(8,128)(2,1)S(1)} %get-tuple-element.59), channel_id=1, source_target_pairs={{0,6},{2,4},{4,2},{6,0},{1,7},{3,5},{5,3},{7,1},{8,14},{10,12},{12... | collective-permute-start | bytes 208904 | tf_op jit(solution)/shard_map/ppermute | solution.py:497
  13.7 5.5 %collective-permute-start.11 = (s16[272,128]{1,0:T(8,128)(2,1)S(1)}, s16[272,128]{1,0:T(8,128)(2,1)S(1)}, u32[]{:S(2)}, u32[]{:S(2)}) collective-permute-start(s16[272,128]{1,0:T(8,128)(2,1)S(1)} %get-tuple-element.60), channel_id=1, source_target_pairs={{0,4},{2,6},{4,0},{6,2},{1,5},{3,7},{5,1},{7,3},{8,12},{10,14},{12... | collective-permute-start | bytes 208904 | tf_op jit(solution)/shard_map/ppermute | solution.py:497
  14.7 11.5 %collective-permute-start.7 = (s16[272,128]{1,0:T(8,128)(2,1)S(1)}, s16[272,128]{1,0:T(8,128)(2,1)S(1)}, u32[]{:S(2)}, u32[]{:S(2)}) collective-permute-start(s16[272,128]{1,0:T(8,128)(2,1)S(1)} %get-tuple-element.56), channel_id=1, source_target_pairs={{0,2},{2,0},{4,6},{6,4},{1,3},{3,1},{5,7},{7,5},{8,10},{10,8},{12,... | collective-permute-start | bytes 208904 | tf_op jit(solution)/shard_map/ppermute | solution.py:497
  16.7 11.4 %collective-permute-start.8 = (s16[272,128]{1,0:T(8,128)(2,1)S(1)}, s16[272,128]{1,0:T(8,128)(2,1)S(1)}, u32[]{:S(2)}, u32[]{:S(2)}) collective-permute-start(s16[272,128]{1,0:T(8,128)(2,1)S(1)} %get-tuple-element.57), channel_id=1, source_target_pairs={{0,4},{2,6},{4,0},{6,2},{1,5},{3,7},{5,1},{7,3},{8,12},{10,14},{12... | collective-permute-start | bytes 208904 | tf_op jit(solution)/shard_map/ppermute | solution.py:497
  18.2 9.9 %collective-permute-start.9 = (s16[272,128]{1,0:T(8,128)(2,1)S(1)}, s16[272,128]{1,0:T(8,128)(2,1)S(1)}, u32[]{:S(2)}, u32[]{:S(2)}) collective-permute-start(s16[272,128]{1,0:T(8,128)(2,1)S(1)} %get-tuple-element.58), channel_id=1, source_target_pairs={{0,6},{2,4},{4,2},{6,0},{1,7},{3,5},{5,3},{7,1},{8,14},{10,12},{12... | collective-permute-start | bytes 208904 | tf_op jit(solution)/shard_map/ppermute | solution.py:497
  19.3 11.4 %collective-permute-start.17 = (s16[272,128]{1,0:T(8,128)(2,1)S(1)}, s16[272,128]{1,0:T(8,128)(2,1)S(1)}, u32[]{:S(2)}, u32[]{:S(2)}) collective-permute-start(s16[272,128]{1,0:T(8,128)(2,1)S(1)} %level_states_0.1.refs_3_), channel_id=1, source_target_pairs={{0,8},{8,16},{16,24},{1,9},{9,17},{17,25},{2,10},{10,18},{18,26},{... | collective-permute-start | bytes 208904 | tf_op jit(solution)/shard_map/ppermute | solution.py:504
  22.8 9.9 %collective-permute-start.16 = (s16[272,128]{1,0:T(8,128)(2,1)S(1)}, s16[272,128]{1,0:T(8,128)(2,1)S(1)}, u32[]{:S(2)}, u32[]{:S(2)}) collective-permute-start(s16[272,128]{1,0:T(8,128)(2,1)S(1)} %level_states_0.1.refs_3_), channel_id=1, source_target_pairs={{0,24},{1,25},{2,26},{3,27},{4,28},{5,29},{6,30},{7,31}} | collective-permute-start | bytes 208904 | tf_op jit(solution)/shard_map/ppermute | solution.py:504
  26.2 6.6 %collective-permute-start.15 = (s16[272,128]{1,0:T(8,128)(2,1)S(1)}, s16[272,128]{1,0:T(8,128)(2,1)S(1)}, u32[]{:S(2)}, u32[]{:S(2)}) collective-permute-start(s16[272,128]{1,0:T(8,128)(2,1)S(1)} %level_states_0.1.refs_3_), channel_id=1, source_target_pairs={{0,16},{8,24},{1,17},{9,25},{2,18},{10,26},{3,19},{11,27},{4,20},{... | collective-permute-start | bytes 208904 | tf_op jit(solution)/shard_map/ppermute | solution.py:504
  28.2 7.6 %collective-permute-start.14 = (s16[272,128]{1,0:T(8,128)(2,1)S(1)}, s16[272,128]{1,0:T(8,128)(2,1)S(1)}, u32[]{:S(2)}, u32[]{:S(2)}) collective-permute-start(s16[272,128]{1,0:T(8,128)(2,1)S(1)} %level_states_1.1.refs_7_), channel_id=1, source_target_pairs={{0,24},{1,25},{2,26},{3,27},{4,28},{5,29},{6,30},{7,31}} | collective-permute-start | bytes 208904 | tf_op jit(solution)/shard_map/ppermute | solution.py:504
  29.5 6.3 %collective-permute-start.13 = (s16[272,128]{1,0:T(8,128)(2,1)S(1)}, s16[272,128]{1,0:T(8,128)(2,1)S(1)}, u32[]{:S(2)}, u32[]{:S(2)}) collective-permute-start(s16[272,128]{1,0:T(8,128)(2,1)S(1)} %level_states_1.1.refs_7_), channel_id=1, source_target_pairs={{0,16},{8,24},{1,17},{9,25},{2,18},{10,26},{3,19},{11,27},{4,20},{... | collective-permute-start | bytes 208904 | tf_op jit(solution)/shard_map/ppermute | solution.py:504
  30.8 5.0 %collective-permute-start.12 = (s16[272,128]{1,0:T(8,128)(2,1)S(1)}, s16[272,128]{1,0:T(8,128)(2,1)S(1)}, u32[]{:S(2)}, u32[]{:S(2)}) collective-permute-start(s16[272,128]{1,0:T(8,128)(2,1)S(1)} %level_states_1.1.refs_7_), channel_id=1, source_target_pairs={{0,8},{8,16},{16,24},{1,9},{9,17},{17,25},{2,10},{10,18},{18,26},{... | collective-permute-start | bytes 208904 | tf_op jit(solution)/shard_map/ppermute | solution.py:504
  33.0 5.3 %collective-permute-start.21 = (s16[272,128]{1,0:T(8,128)(2,1)S(1)}, s16[272,128]{1,0:T(8,128)(2,1)S(1)}, u32[]{:S(2)}, u32[]{:S(2)}) collective-permute-start(s16[272,128]{1,0:T(8,128)(2,1)S(1)} %get-tuple-element.65), channel_id=1, source_target_pairs={{0,6},{2,4},{4,2},{6,0},{1,7},{3,5},{5,3},{7,1},{8,14},{10,12},{12... | collective-permute-start | bytes 208904 | tf_op jit(solution)/shard_map/ppermute | solution.py:497
  34.8 4.6 %collective-permute-start.20 = (s16[272,128]{1,0:T(8,128)(2,1)S(1)}, s16[272,128]{1,0:T(8,128)(2,1)S(1)}, u32[]{:S(2)}, u32[]{:S(2)}) collective-permute-start(s16[272,128]{1,0:T(8,128)(2,1)S(1)} %get-tuple-element.61.refs_7_), channel_id=1, source_target_pairs={{0,2},{2,0},{4,6},{6,4},{1,3},{3,1},{5,7},{7,5},{8,10},{10,8},{12,... | collective-permute-start | bytes 208904 | tf_op jit(solution)/shard_map/ppermute | solution.py:497
  36.0 6.0 %collective-permute-start.19 = (s16[272,128]{1,0:T(8,128)(2,1)S(1)}, s16[272,128]{1,0:T(8,128)(2,1)S(1)}, u32[]{:S(2)}, u32[]{:S(2)}) collective-permute-start(s16[272,128]{1,0:T(8,128)(2,1)S(1)} %get-tuple-element.63), channel_id=1, source_target_pairs={{0,6},{2,4},{4,2},{6,0},{1,7},{3,5},{5,3},{7,1},{8,14},{10,12},{12... | collective-permute-start | bytes 208904 | tf_op jit(solution)/shard_map/ppermute | solution.py:497
  37.8 5.1 %collective-permute-start.18 = (s16[272,128]{1,0:T(8,128)(2,1)S(1)}, s16[272,128]{1,0:T(8,128)(2,1)S(1)}, u32[]{:S(2)}, u32[]{:S(2)}) collective-permute-start(s16[272,128]{1,0:T(8,128)(2,1)S(1)} %get-tuple-element.62.refs_10_), channel_id=1, source_target_pairs={{0,2},{2,0},{4,6},{6,4},{1,3},{3,1},{5,7},{7,5},{8,10},{10,8},{12,... | collective-permute-start | bytes 208904 | tf_op jit(solution)/shard_map/ppermute | solution.py:497
  40.7 16.6 %collective-permute-start.24 = (bf16[512,512]{1,0:T(8,128)(2,1)S(1)}, bf16[512,512]{1,0:T(8,128)(2,1)S(1)}, u32[]{:S(2)}, u32[]{:S(2)}) collective-permute-start(bf16[512,512]{1,0:T(8,128)(2,1)S(1)} %attend_0_1_3.1.refs_10_), channel_id=1, source_target_pairs={{0,2},{2,0},{1,3},{3,1},{4,6},{6,4},{5,7},{7,5},{8,10},{10,8},{9,1... | collective-permute-start | bytes 1572872 | tf_op jit(solution)/shard_map/ppermute | solution.py:497
  44.3 19.2 %collective-permute-start.22 = (bf16[512,512]{1,0:T(8,128)(2,1)S(1)}, bf16[512,512]{1,0:T(8,128)(2,1)S(1)}, u32[]{:S(2)}, u32[]{:S(2)}) collective-permute-start(bf16[512,512]{1,0:T(8,128)(2,1)S(1)} %attend_1_1_3.1.refs_14_.refs_10_), channel_id=1, source_target_pairs={{0,2},{2,0},{1,3},{3,1},{4,6},{6,4},{5,7},{7,5},{8,10},{10,8},{9,1... | collective-permute-start | bytes 1572872 | tf_op jit(solution)/shard_map/ppermute | solution.py:497
  45.9 10.6 %collective-permute-start.25 = (f32[2,2,128,128]{3,2,1,0:T(8,128)S(1)}, f32[2,2,128,128]{3,2,1,0:T(8,128)S(1)}, u32[]{:S(2)}, u32[]{:S(2)}) collective-permute-start(f32[2,2,128,128]{3,2,1,0:T(8,128)S(1)} %get-tuple-element.69), channel_id=1, source_target_pairs={{0,4},{4,0},{1,5},{5,1},{2,6},{6,2},{3,7},{7,3},{8,12},{12,8},{9,1... | collective-permute-start | bytes 786440 | tf_op jit(solution)/shard_map/ppermute | solution.py:497
  47.3 6.5 %collective-permute-start.23 = (s16[528,128]{1,0:T(8,128)(2,1)S(1)}, s16[528,128]{1,0:T(8,128)(2,1)S(1)}, u32[]{:S(2)}, u32[]{:S(2)}) collective-permute-start(s16[528,128]{1,0:T(8,128)(2,1)S(1)} %get-tuple-element.67), channel_id=1, source_target_pairs={{0,4},{2,6},{4,0},{6,2},{1,5},{3,7},{5,1},{7,3},{8,12},{10,14},{12... | collective-permute-start | bytes 405512 | tf_op jit(solution)/shard_map/ppermute | solution.py:497

commit v18 on v16

--- a/solution.py
+++ b/solution.py
@@ -128,23 +128,23 @@
     )(spikes, keys, values)
 
 
-def spike_queries(plan, queries, counts):
+def spike_queries(plan, queries, counts, after):
     n = len(counts)
 
     def kernel(place_ref, queries_ref, *refs):
         for side, half, mine, columns in sides(plan, place_ref[0]):
             at = side * plan.halves + half
-            refs[n + at][:, mine] = queries_ref[:, columns] * refs[at][:, mine]
+            refs[n + len(after) + at][:, mine] = queries_ref[:, columns] * refs[at][:, mine]
 
     return pl.pallas_call(
         at_place(kernel),
         out_shape=[jax.ShapeDtypeStruct(a.shape, jnp.bfloat16) for a in counts],
-        in_specs=[VMEM] * (1 + n),
+        in_specs=[VMEM] * (1 + n) + [ANY] * len(after),
         out_specs=[VMEM] * n,
         compiler_params=params(),
         cost_estimate=cost(queries.size, queries.size * 6),
         name="spike_queries",
-    )(queries, *counts)
+    )(queries, *counts, *after)
 
 
 def contract_rows(left, right):
@@ -503,8 +503,7 @@
         return [(a, swap(b, "core", 1, CORES)) for a, b in zip(mine, theirs)]
 
     key, value = with_siblings(*parts[0:2]), with_siblings(*parts[2:4])
-    spiked = spike_queries(plan, queries, [*parts[4], *parts[5]])
-    query = with_siblings(spiked[: plan.halves], spiked[plan.halves :])
+    counts = [*parts[4], *parts[5]]
 
     own, first, others = [], [], []
 
@@ -547,10 +546,13 @@
             after = [part]
         return after
 
-    after = [query[0][0]]
+    after = []
     for half in halves:
         owner_stage(half, after)
-        after = [own[-1], *[a for _, a in query]]
+        if half == 0:
+            spiked = spike_queries(plan, queries, counts, [own[0]])
+            query = with_siblings(spiked[: plan.halves], spiked[plan.halves :])
+        after = [own[-1], *[b for _, b in query]]
     levels = []
     for half in halves:
         level = level_states(plan, own[half], others[half][::-1], half, after)

time: 63.5 us -> 64.2 us (1.011)
  waiting for transfers between devices: 13.5 us -> 14.7 us
    ppermute x20, waiting for transfers between devices: 13.5 us -> 14.7 us  [swap(): return lax.ppermute(array, axes, [(i, i ^ offset) for i in range(size)])]
  transfers between devices with their start and end apart: 26 -> 26, of which waited for: 6 -> 6; matrix products, arithmetic and copies ran while one was open for 0% -> 0% of each run, Pallas kernels for 17% -> 16%
where the time goes in v18:
time: 64.2 us; the launch traced here: 63.9 us
  starting transfers between devices  33.4 us (52%)
  Pallas kernels  15 us (23%)
  waiting for transfers between devices  14.7 us (23%)
  between operations  0.86 us (1%)
    ppermute x20, starting transfers between devices, swap(): return lax.ppermute(array, axes, [(i, i ^ offset) for i in range(size)])  20.2 us
    ppermute x20, waiting for transfers between devices, swap(): return lax.ppermute(array, axes, [(i, i ^ offset) for i in range(size)])  14.7 us
    ppermute x6, starting transfers between devices, to_later(): return lax.ppermute(array, 'outer', pairs)  13.2 us
    pallas_call x4, Pallas kernels, attend(): pl.pallas_call(at_place(kernel), out_shape=jax.ShapeDtypeStruct((CORES *...  5.3 us
    pallas_call x1, Pallas kernels, decode(): pl.pallas_call(kernel, out_shape=[jax.ShapeDtypeStruct((rows, plan.n_y *...  3.74 us
    pallas_call x2, Pallas kernels, assemble(): pl.pallas_call(at_place(kernel), out_shape=jax.ShapeDtypeStruct((plan.n_y...  1.99 us
    pallas_call x2, Pallas kernels, chunk_states(): pl.pallas_call(at_place(kernel), out_shape=[states_shape(plan.each), stat...  1.64 us
  transfers between devices with their start and end apart: 26, of which 6 were waited for; matrix products, arithmetic and copies ran while one was open for 0% of the time, Pallas kernels for 16%

profile of v18, /device:TPU:0, one launch (start us, length us, event | category | flops | bytes accessed | tf_op | source)
XLA Modules:
  0.0 63.9 jit_solution(7489045102846565195)
XLA Ops:
  0.6 3.7 %decode.1 = (bf16[256,1024]{1,0:T(8,128)(2,1)S(1)}, bf16[256,1024]{1,0:T(8,128)(2,1)S(1)}, bf16[256,1024]{1,0:T(8,128)(2,1)S(1)}, bf16[256,1024]{1,0:T(8,128)(2,...) custom-call(s32[256,4096]{1,0:T(8,128)} %refs_0_.2, ...), custom_call_target="tpu_custom_call" | custom-call | flops 4194304 | bytes 14680064 | tf_op jit(solution)/shard_map/decode/pallas_call | solution.py:114
  4.4 0.0 copy-start
  4.4 0.5 collective-permute-start
  4.9 0.1 collective-permute-start.1
  5.0 0.4 collective-permute-start.3
  5.4 0.1 collective-permute-start.4
  5.5 0.9 %collective-permute-done.refs_1_.refs_3_ = bf16[256,1024]{1,0:T(8,128)(2,1)S(1)} collective-permute-done((bf16[256,1024]{1,0:T(8,128)(2,1)S(1)}, bf16[256,1024]{1,0:T(8,128)(2,1)S(1)}, u32[]{:S(2)}, u32[]{:S(2)}) %collective-permute-start) | collective-permute-done | bytes 524320 | tf_op jit(solution)/shard_map/ppermute | solution.py:489
  6.5 0.7 %collective-permute-done.1.refs_3_.refs_5_ = bf16[256,1024]{1,0:T(8,128)(2,1)S(1)} collective-permute-done((bf16[256,1024]{1,0:T(8,128)(2,1)S(1)}, bf16[256,1024]{1,0:T(8,128)(2,1)S(1)}, u32[]{:S(2)}, u32[]{:S(2)}) %collective-permute-start.1) | collective-permute-done | bytes 524320 | tf_op jit(solution)/shard_map/ppermute | solution.py:489
  7.2 0.8 %chunk_states_0.1 = (f32[2,128,128]{2,1,0:T(8,128)S(1)}, f32[4,2,128,128]{3,2,1,0:T(8,128)S(1)}, s16[288,128]{1,0:T(8,128)(2,1)S(1)}, s16[272,128]{1,0:T(8,128)(2,1)S(1)}, s16[272,128]{1,0:T(8,128)(2,1)S(1)}) custom-call(bf16[256,1024]{1,0:T(8,128)(2,1)S(1)} %get-tuple-element.40.refs_0_.refs_2_, bf16[256,1024]{1,0:T(8,128)(2,1)S(1)} %collective-permute-done.refs_1_.refs_3_, ...), custom_call_target="tpu_custom_call" | custom-call | flops 134217728 | bytes 2883584 | tf_op jit(solution)/shard_map/chunk_states_0/pallas_call | solution.py:251
  8.0 0.3 spike_queries.1
  8.3 0.4 collective-permute-start.2
  8.8 0.1 collective-permute-start.5
  8.9 2.9 %collective-permute-start.6 = (s16[288,128]{1,0:T(8,128)(2,1)S(1)}, s16[288,128]{1,0:T(8,128)(2,1)S(1)}, u32[]{:S(2)}, u32[]{:S(2)}) collective-permute-start(s16[288,128]{1,0:T(8,128)(2,1)S(1)} %get-tuple-element.53), channel_id=1, source_target_pairs={{0,2},{2,0},{4,6},{6,4},{1,3},{3,1},{5,7},{7,5},{8,10},{10,8},{12,... | collective-permute-start | bytes 221192 | tf_op jit(solution)/shard_map/ppermute | solution.py:489
  11.8 0.0 collective-permute-done.3.refs_1_.refs_3_
  11.8 1.4 %collective-permute-start.10 = (s16[272,128]{1,0:T(8,128)(2,1)S(1)}, s16[272,128]{1,0:T(8,128)(2,1)S(1)}, u32[]{:S(2)}, u32[]{:S(2)}) collective-permute-start(s16[272,128]{1,0:T(8,128)(2,1)S(1)} %get-tuple-element.58), channel_id=1, source_target_pairs={{0,6},{2,4},{4,2},{6,0},{1,7},{3,5},{5,3},{7,1},{8,14},{10,12},{12... | collective-permute-start | bytes 208904 | tf_op jit(solution)/shard_map/ppermute | solution.py:489
  13.2 0.0 collective-permute-done.4.refs_3_.refs_5_
  13.2 0.1 collective-permute-start.11
  13.4 0.0 collective-permute-done.2.refs_6_.refs_5_.refs_1_
  13.4 0.0 collective-permute-done.5.refs_5_.refs_4_.refs_1_
  13.4 0.8 %chunk_states_1.1 = (f32[2,128,128]{2,1,0:T(8,128)S(1)}, f32[4,2,128,128]{3,2,1,0:T(8,128)S(1)}, s16[272,128]{1,0:T(8,128)(2,1)S(1)}, s16[272,128]{1,0:T(8,128)(2,1)S(1)}, s16[272,128]{1,0:T(8,128)(2,1)S(1)}) custom-call(bf16[256,1024]{1,0:T(8,128)(2,1)S(1)} %get-tuple-element.47.refs_0_.refs_2_, ...), custom_call_target="tpu_custom_call" | custom-call | flops 134217728 | bytes 2883584 | tf_op jit(solution)/shard_map/chunk_states_1/pallas_call | solution.py:251
  14.2 2.0 %collective-permute-start.7 = (s16[272,128]{1,0:T(8,128)(2,1)S(1)}, s16[272,128]{1,0:T(8,128)(2,1)S(1)}, u32[]{:S(2)}, u32[]{:S(2)}) collective-permute-start(s16[272,128]{1,0:T(8,128)(2,1)S(1)} %get-tuple-element.55), channel_id=1, source_target_pairs={{0,2},{2,0},{4,6},{6,4},{1,3},{3,1},{5,7},{7,5},{8,10},{10,8},{12,... | collective-permute-start | bytes 208904 | tf_op jit(solution)/shard_map/ppermute | solution.py:489
  16.2 1.5 %collective-permute-start.8 = (s16[272,128]{1,0:T(8,128)(2,1)S(1)}, s16[272,128]{1,0:T(8,128)(2,1)S(1)}, u32[]{:S(2)}, u32[]{:S(2)}) collective-permute-start(s16[272,128]{1,0:T(8,128)(2,1)S(1)} %get-tuple-element.56), channel_id=1, source_target_pairs={{0,4},{2,6},{4,0},{6,2},{1,5},{3,7},{5,1},{7,3},{8,12},{10,14},{12... | collective-permute-start | bytes 208904 | tf_op jit(solution)/shard_map/ppermute | solution.py:489
  17.7 0.0 collective-permute-done.10.refs_0_.refs_3_
  17.7 1.1 %collective-permute-start.9 = (s16[272,128]{1,0:T(8,128)(2,1)S(1)}, s16[272,128]{1,0:T(8,128)(2,1)S(1)}, u32[]{:S(2)}, u32[]{:S(2)}) collective-permute-start(s16[272,128]{1,0:T(8,128)(2,1)S(1)} %get-tuple-element.57), channel_id=1, source_target_pairs={{0,6},{2,4},{4,2},{6,0},{1,7},{3,5},{5,3},{7,1},{8,14},{10,12},{12... | collective-permute-start | bytes 208904 | tf_op jit(solution)/shard_map/ppermute | solution.py:489
  18.8 0.0 collective-permute-done.6.refs_2_.refs_1_.refs_7_
  18.8 0.1 level_states_0.1.refs_3_
  18.9 3.5 %collective-permute-start.17 = (s16[272,128]{1,0:T(8,128)(2,1)S(1)}, s16[272,128]{1,0:T(8,128)(2,1)S(1)}, u32[]{:S(2)}, u32[]{:S(2)}) collective-permute-start(s16[272,128]{1,0:T(8,128)(2,1)S(1)} %level_states_0.1.refs_3_), channel_id=1, source_target_pairs={{0,8},{8,16},{16,24},{1,9},{9,17},{17,25},{2,10},{10,18},{18,26},{... | collective-permute-start | bytes 208904 | tf_op jit(solution)/shard_map/ppermute | solution.py:496
  22.4 3.3 %collective-permute-start.16 = (s16[272,128]{1,0:T(8,128)(2,1)S(1)}, s16[272,128]{1,0:T(8,128)(2,1)S(1)}, u32[]{:S(2)}, u32[]{:S(2)}) collective-permute-start(s16[272,128]{1,0:T(8,128)(2,1)S(1)} %level_states_0.1.refs_3_), channel_id=1, source_target_pairs={{0,24},{1,25},{2,26},{3,27},{4,28},{5,29},{6,30},{7,31}} | collective-permute-start | bytes 208904 | tf_op jit(solution)/shard_map/ppermute | solution.py:496
  25.8 1.8 %collective-permute-start.15 = (s16[272,128]{1,0:T(8,128)(2,1)S(1)}, s16[272,128]{1,0:T(8,128)(2,1)S(1)}, u32[]{:S(2)}, u32[]{:S(2)}) collective-permute-start(s16[272,128]{1,0:T(8,128)(2,1)S(1)} %level_states_0.1.refs_3_), channel_id=1, source_target_pairs={{0,16},{8,24},{1,17},{9,25},{2,18},{10,26},{3,19},{11,27},{4,20},{... | collective-permute-start | bytes 208904 | tf_op jit(solution)/shard_map/ppermute | solution.py:496
  27.6 0.0 collective-permute-done.8.refs_1_.refs_2_.refs_9_
  27.6 0.0 collective-permute-done.9.refs_0_.refs_3_.refs_10_
  27.6 0.1 level_states_1.1.refs_7_
  27.7 1.3 %collective-permute-start.14 = (s16[272,128]{1,0:T(8,128)(2,1)S(1)}, s16[272,128]{1,0:T(8,128)(2,1)S(1)}, u32[]{:S(2)}, u32[]{:S(2)}) collective-permute-start(s16[272,128]{1,0:T(8,128)(2,1)S(1)} %level_states_1.1.refs_7_), channel_id=1, source_target_pairs={{0,24},{1,25},{2,26},{3,27},{4,28},{5,29},{6,30},{7,31}} | collective-permute-start | bytes 208904 | tf_op jit(solution)/shard_map/ppermute | solution.py:496
  29.0 1.3 %collective-permute-start.13 = (s16[272,128]{1,0:T(8,128)(2,1)S(1)}, s16[272,128]{1,0:T(8,128)(2,1)S(1)}, u32[]{:S(2)}, u32[]{:S(2)}) collective-permute-start(s16[272,128]{1,0:T(8,128)(2,1)S(1)} %level_states_1.1.refs_7_), channel_id=1, source_target_pairs={{0,16},{8,24},{1,17},{9,25},{2,18},{10,26},{3,19},{11,27},{4,20},{... | collective-permute-start | bytes 208904 | tf_op jit(solution)/shard_map/ppermute | solution.py:496
  30.4 2.0 %collective-permute-start.12 = (s16[272,128]{1,0:T(8,128)(2,1)S(1)}, s16[272,128]{1,0:T(8,128)(2,1)S(1)}, u32[]{:S(2)}, u32[]{:S(2)}) collective-permute-start(s16[272,128]{1,0:T(8,128)(2,1)S(1)} %level_states_1.1.refs_7_), channel_id=1, source_target_pairs={{0,8},{8,16},{16,24},{1,9},{9,17},{17,25},{2,10},{10,18},{18,26},{... | collective-permute-start | bytes 208904 | tf_op jit(solution)/shard_map/ppermute | solution.py:496
  32.3 0.0 collective-permute-done.16.refs_5_
  32.3 0.2 carries_0.1
  32.6 1.8 %collective-permute-start.21 = (s16[272,128]{1,0:T(8,128)(2,1)S(1)}, s16[272,128]{1,0:T(8,128)(2,1)S(1)}, u32[]{:S(2)}, u32[]{:S(2)}) collective-permute-start(s16[272,128]{1,0:T(8,128)(2,1)S(1)} %get-tuple-element.65), channel_id=1, source_target_pairs={{0,6},{2,4},{4,2},{6,0},{1,7},{3,5},{5,3},{7,1},{8,14},{10,12},{12... | collective-permute-start | bytes 208904 | tf_op jit(solution)/shard_map/ppermute | solution.py:489
  34.4 1.0 %collective-permute-start.20 = (s16[272,128]{1,0:T(8,128)(2,1)S(1)}, s16[272,128]{1,0:T(8,128)(2,1)S(1)}, u32[]{:S(2)}, u32[]{:S(2)}) collective-permute-start(s16[272,128]{1,0:T(8,128)(2,1)S(1)} %get-tuple-element.60.refs_7_), channel_id=1, source_target_pairs={{0,2},{2,0},{4,6},{6,4},{1,3},{3,1},{5,7},{7,5},{8,10},{10,8},{12,... | collective-permute-start | bytes 208904 | tf_op jit(solution)/shard_map/ppermute | solution.py:489
  35.4 0.0 collective-permute-done.14.refs_6_.refs_13_
  35.4 0.0 collective-permute-done.13.refs_5_.refs_12_
  35.4 0.0 collective-permute-done.12.refs_4_.refs_11_
  35.4 0.2 carries_1.1
  35.6 1.8 %collective-permute-start.19 = (s16[272,128]{1,0:T(8,128)(2,1)S(1)}, s16[272,128]{1,0:T(8,128)(2,1)S(1)}, u32[]{:S(2)}, u32[]{:S(2)}) collective-permute-start(s16[272,128]{1,0:T(8,128)(2,1)S(1)} %get-tuple-element.62), channel_id=1, source_target_pairs={{0,6},{2,4},{4,2},{6,0},{1,7},{3,5},{5,3},{7,1},{8,14},{10,12},{12... | collective-permute-start | bytes 208904 | tf_op jit(solution)/shard_map/ppermute | solution.py:489
  37.4 0.4 collective-permute-start.18
  37.9 0.0 collective-permute-done.21.refs_9_
  37.9 1.1 %collective-permute-done.20.refs_8_ = s16[272,128]{1,0:T(8,128)(2,1)S(1)} collective-permute-done((s16[272,128]{1,0:T(8,128)(2,1)S(1)}, s16[272,128]{1,0:T(8,128)(2,1)S(1)}, u32[]{:S(2)}, u32[]{:S(2)}) %collective-permute-start.20) | collective-permute-done | bytes 69664 | tf_op jit(solution)/shard_map/ppermute | solution.py:489
  39.0 1.3 %attend_0_1_3.1.refs_10_ = bf16[512,512]{1,0:T(8,128)(2,1)S(1)} custom-call(bf16[256,1024]{1,0:T(8,128)(2,1)S(1)} %get-tuple-element.63.refs_0_, bf16[256,1024]{1,0:T(8,128)(2,1)S(1)} %collective-permute-done.5.refs_5_.refs_4_.refs_1_, bf16[256,1024]{1,0:T(8,128)(2,1)S(1)} %get-tuple-element.40.refs_0_.refs_2_, ...), custom_call_target="tpu_custom_call" | custom-call | flops 402653184 | bytes 2097152 | tf_op jit(solution)/shard_map/attend_0_1_3/pallas_call | solution.py:415
  40.3 1.2 %collective-permute-start.24 = (bf16[512,512]{1,0:T(8,128)(2,1)S(1)}, bf16[512,512]{1,0:T(8,128)(2,1)S(1)}, u32[]{:S(2)}, u32[]{:S(2)}) collective-permute-start(bf16[512,512]{1,0:T(8,128)(2,1)S(1)} %attend_0_1_3.1.refs_10_), channel_id=1, source_target_pairs={{0,2},{2,0},{1,3},{3,1},{4,6},{6,4},{5,7},{7,5},{8,10},{10,8},{9,1... | collective-permute-start | bytes 1572872 | tf_op jit(solution)/shard_map/ppermute | solution.py:489
  41.6 0.0 collective-permute-done.19.refs_9_
  41.6 1.0 %collective-permute-done.18.refs_8_ = s16[272,128]{1,0:T(8,128)(2,1)S(1)} collective-permute-done((s16[272,128]{1,0:T(8,128)(2,1)S(1)}, s16[272,128]{1,0:T(8,128)(2,1)S(1)}, u32[]{:S(2)}, u32[]{:S(2)}) %collective-permute-start.18) | collective-permute-done | bytes 69664 | tf_op jit(solution)/shard_map/ppermute | solution.py:489
  42.6 1.3 %attend_1_1_3.1.refs_14_.refs_10_ = bf16[512,512]{1,0:T(8,128)(2,1)S(1)} custom-call(bf16[256,1024]{1,0:T(8,128)(2,1)S(1)} %get-tuple-element.45.refs_0_, bf16[256,1024]{1,0:T(8,128)(2,1)S(1)} %collective-permute-done.2.refs_6_.refs_5_.refs_1_, bf16[256,1024]{1,0:T(8,128)(2,1)S(1)} %get-tuple-element.47.refs_0_.refs_2_, ...), custom_call_target="tpu_custom_call" | custom-call | flops 402653184 | bytes 2097152 | tf_op jit(solution)/shard_map/attend_1_1_3/pallas_call | solution.py:415
  43.9 1.0 %collective-permute-start.22 = (bf16[512,512]{1,0:T(8,128)(2,1)S(1)}, bf16[512,512]{1,0:T(8,128)(2,1)S(1)}, u32[]{:S(2)}, u32[]{:S(2)}) collective-permute-start(bf16[512,512]{1,0:T(8,128)(2,1)S(1)} %attend_1_1_3.1.refs_14_.refs_10_), channel_id=1, source_target_pairs={{0,2},{2,0},{1,3},{3,1},{4,6},{6,4},{5,7},{7,5},{8,10},{10,8},{9,1... | collective-permute-start | bytes 1572872 | tf_op jit(solution)/shard_map/ppermute | solution.py:489
  44.9 0.6 own_carries.1
  45.5 1.4 %collective-permute-start.25 = (f32[2,2,128,128]{3,2,1,0:T(8,128)S(1)}, f32[2,2,128,128]{3,2,1,0:T(8,128)S(1)}, u32[]{:S(2)}, u32[]{:S(2)}) collective-permute-start(f32[2,2,128,128]{3,2,1,0:T(8,128)S(1)} %get-tuple-element.69), channel_id=1, source_target_pairs={{0,4},{4,0},{1,5},{5,1},{2,6},{6,2},{3,7},{7,3},{8,12},{12,8},{9,1... | collective-permute-start | bytes 786440 | tf_op jit(solution)/shard_map/ppermute | solution.py:489
  46.9 0.7 %collective-permute-start.23 = (s16[528,128]{1,0:T(8,128)(2,1)S(1)}, s16[528,128]{1,0:T(8,128)(2,1)S(1)}, u32[]{:S(2)}, u32[]{:S(2)}) collective-permute-start(s16[528,128]{1,0:T(8,128)(2,1)S(1)} %get-tuple-element.67), channel_id=1, source_target_pairs={{0,4},{2,6},{4,0},{6,2},{1,5},{3,7},{5,1},{7,3},{8,12},{10,14},{12... | collective-permute-start | bytes 405512 | tf_op jit(solution)/shard_map/ppermute | solution.py:489
  47.6 5.8 %collective-permute-done.23.refs_9_ = s16[528,128]{1,0:T(8,128)(2,1)S(1)} collective-permute-done((s16[528,128]{1,0:T(8,128)(2,1)S(1)}, s16[528,128]{1,0:T(8,128)(2,1)S(1)}, u32[]{:S(2)}, u32[]{:S(2)}) %collective-permute-start.23) | collective-permute-done | bytes 135200 | tf_op jit(solution)/shard_map/ppermute | solution.py:489
  53.3 1.3 %attend_0_0_2.1.refs_10_.refs_0_ = bf16[512,512]{1,0:T(8,128)(2,1)S(1)} custom-call(bf16[256,1024]{1,0:T(8,128)(2,1)S(1)} %get-tuple-element.63.refs_0_, bf16[256,1024]{1,0:T(8,128)(2,1)S(1)} %collective-permute-done.5.refs_5_.refs_4_.refs_1_, bf16[256,1024]{1,0:T(8,128)(2,1)S(1)} %get-tuple-element.40.refs_0_.refs_2_, ...), custom_call_target="tpu_custom_call" | custom-call | flops 402653184 | bytes 2097152 | tf_op jit(solution)/shard_map/attend_0_0_2/pallas_call | solution.py:415
  54.7 1.3 %attend_1_0_2.1.refs_1_ = bf16[512,512]{1,0:T(8,128)(2,1)S(1)} custom-call(bf16[256,1024]{1,0:T(8,128)(2,1)S(1)} %get-tuple-element.45.refs_0_, bf16[256,1024]{1,0:T(8,128)(2,1)S(1)} %collective-permute-done.2.refs_6_.refs_5_.refs_1_, bf16[256,1024]{1,0:T(8,128)(2,1)S(1)} %get-tuple-element.47.refs_0_.refs_2_, ...), custom_call_target="tpu_custom_call" | custom-call | flops 402653184 | bytes 2097152 | tf_op jit(solution)/shard_map/attend_1_0_2/pallas_call | solution.py:415
  56.0 0.0 collective-permute-done.25.refs_1_
  56.0 0.8 %assemble_cache.1 = f32[1,8,128,128]{3,2,1,0:T(8,128)} custom-call(f32[2,2,128,128]{3,2,1,0:T(8,128)S(1)} %get-tuple-element.68.refs_0_, f32[2,2,128,128]{3,2,1,0:T(8,128)S(1)} %collective-permute-done.25.refs_1_), custom_call_target="tpu_custom_call" | custom-call | tf_op jit(solution)/shard_map/assemble_cache/pallas_call | solution.py:475
  56.9 1.2 %assemble.1.refs_1_ = bf16[1024,1024]{1,0:T(8,128)(2,1)} custom-call(bf16[512,512]{1,0:T(8,128)(2,1)S(1)} %attend_0_0_2.1.refs_10_.refs_0_, bf16[512,512]{1,0:T(8,128)(2,1)S(1)} %attend_1_0_2.1.refs_1_, bf16[512,512]{1,0:T(8,128)(2,1)S(1)} %collective-permute-done.24.refs_2_), custom_call_target="tpu_custom_call" | custom-call | tf_op jit(solution)/shard_map/assemble/pallas_call | solution.py:454
  58.1 5.1 %collective-permute-done.22.refs_0_ = bf16[512,512]{1,0:T(8,128)(2,1)S(1)} collective-permute-done((bf16[512,512]{1,0:T(8,128)(2,1)S(1)}, bf16[512,512]{1,0:T(8,128)(2,1)S(1)}, u32[]{:S(2)}, u32[]{:S(2)}) %collective-permute-start.22) | collective-permute-done | bytes 524320 | tf_op jit(solution)/shard_map/ppermute | solution.py:489
  63.1 0.8 %finish.1 = bf16[1024,1024]{1,0:T(8,128)(2,1)} custom-call(bf16[512,512]{1,0:T(8,128)(2,1)S(1)} %collective-permute-done.22.refs_0_, bf16[1024,1024]{1,0:T(8,128)(2,1)} %assemble.1.refs_1_), custom_call_target="tpu_custom_call", output_to_operand_aliasing={{}: (1, {})} | custom-call | tf_op jit(solution)/shard_map/finish/pallas_call | solution.py:454
  (8 shorter events, 0.0 us)
Async XLA Ops:
  0.6 6.6 %copy-start.1 = (f32[1024]{0:T(1024)S(1)}, f32[1024]{0:T(1024)}, u32[]{:S(2)}) copy-start(f32[1024]{0:T(1024)} %param.9) | copy-start | bytes 12292
  4.4 3.6 %copy-start = (bf16[256,4096]{1,0:T(8,128)(2,1)S(1)}, bf16[256,4096]{1,0:T(8,128)(2,1)}, u32[]{:S(2)}) copy-start(bf16[256,4096]{1,0:T(8,128)(2,1)} %refs_0_.3) | copy-start | bytes 6291460
  4.4 2.1 %collective-permute-start = (bf16[256,1024]{1,0:T(8,128)(2,1)S(1)}, bf16[256,1024]{1,0:T(8,128)(2,1)S(1)}, u32[]{:S(2)}, u32[]{:S(2)}) collective-permute-start(bf16[256,1024]{1,0:T(8,128)(2,1)S(1)} %get-tuple-element.41), channel_id=1, source_target_pairs={{0,1},{1,0},{2,3},{3,2},{4,5},{5,4},{6,7},{7,6},{8,9},{9,8},{10,11... | collective-permute-start | bytes 1572872 | tf_op jit(solution)/shard_map/ppermute | solution.py:489
  4.9 2.3 %collective-permute-start.1 = (bf16[256,1024]{1,0:T(8,128)(2,1)S(1)}, bf16[256,1024]{1,0:T(8,128)(2,1)S(1)}, u32[]{:S(2)}, u32[]{:S(2)}) collective-permute-start(bf16[256,1024]{1,0:T(8,128)(2,1)S(1)} %get-tuple-element.43), channel_id=1, source_target_pairs={{0,1},{1,0},{2,3},{3,2},{4,5},{5,4},{6,7},{7,6},{8,9},{9,8},{10,11... | collective-permute-start | bytes 1572872 | tf_op jit(solution)/shard_map/ppermute | solution.py:489
  5.0 6.8 %collective-permute-start.3 = (bf16[256,1024]{1,0:T(8,128)(2,1)S(1)}, bf16[256,1024]{1,0:T(8,128)(2,1)S(1)}, u32[]{:S(2)}, u32[]{:S(2)}) collective-permute-start(bf16[256,1024]{1,0:T(8,128)(2,1)S(1)} %get-tuple-element.48), channel_id=1, source_target_pairs={{0,1},{1,0},{2,3},{3,2},{4,5},{5,4},{6,7},{7,6},{8,9},{9,8},{10,11... | collective-permute-start | bytes 1572872 | tf_op jit(solution)/shard_map/ppermute | solution.py:489
  5.4 7.8 %collective-permute-start.4 = (bf16[256,1024]{1,0:T(8,128)(2,1)S(1)}, bf16[256,1024]{1,0:T(8,128)(2,1)S(1)}, u32[]{:S(2)}, u32[]{:S(2)}) collective-permute-start(bf16[256,1024]{1,0:T(8,128)(2,1)S(1)} %get-tuple-element.50), channel_id=1, source_target_pairs={{0,1},{1,0},{2,3},{3,2},{4,5},{5,4},{6,7},{7,6},{8,9},{9,8},{10,11... | collective-permute-start | bytes 1572872 | tf_op jit(solution)/shard_map/ppermute | solution.py:489
  8.3 5.0 %collective-permute-start.2 = (bf16[256,1024]{1,0:T(8,128)(2,1)S(1)}, bf16[256,1024]{1,0:T(8,128)(2,1)S(1)}, u32[]{:S(2)}, u32[]{:S(2)}) collective-permute-start(bf16[256,1024]{1,0:T(8,128)(2,1)S(1)} %get-tuple-element.46), channel_id=1, source_target_pairs={{0,1},{1,0},{2,3},{3,2},{4,5},{5,4},{6,7},{7,6},{8,9},{9,8},{10,11... | collective-permute-start | bytes 1572872 | tf_op jit(solution)/shard_map/ppermute | solution.py:489
  8.8 4.6 %collective-permute-start.5 = (bf16[256,1024]{1,0:T(8,128)(2,1)S(1)}, bf16[256,1024]{1,0:T(8,128)(2,1)S(1)}, u32[]{:S(2)}, u32[]{:S(2)}) collective-permute-start(bf16[256,1024]{1,0:T(8,128)(2,1)S(1)} %get-tuple-element.51), channel_id=1, source_target_pairs={{0,1},{1,0},{2,3},{3,2},{4,5},{5,4},{6,7},{7,6},{8,9},{9,8},{10,11... | collective-permute-start | bytes 1572872 | tf_op jit(solution)/shard_map/ppermute | solution.py:489
  8.9 9.9 %collective-permute-start.6 = (s16[288,128]{1,0:T(8,128)(2,1)S(1)}, s16[288,128]{1,0:T(8,128)(2,1)S(1)}, u32[]{:S(2)}, u32[]{:S(2)}) collective-permute-start(s16[288,128]{1,0:T(8,128)(2,1)S(1)} %get-tuple-element.53), channel_id=1, source_target_pairs={{0,2},{2,0},{4,6},{6,4},{1,3},{3,1},{5,7},{7,5},{8,10},{10,8},{12,... | collective-permute-start | bytes 221192 | tf_op jit(solution)/shard_map/ppermute | solution.py:489
  11.8 5.9 %collective-permute-start.10 = (s16[272,128]{1,0:T(8,128)(2,1)S(1)}, s16[272,128]{1,0:T(8,128)(2,1)S(1)}, u32[]{:S(2)}, u32[]{:S(2)}) collective-permute-start(s16[272,128]{1,0:T(8,128)(2,1)S(1)} %get-tuple-element.58), channel_id=1, source_target_pairs={{0,6},{2,4},{4,2},{6,0},{1,7},{3,5},{5,3},{7,1},{8,14},{10,12},{12... | collective-permute-start | bytes 208904 | tf_op jit(solution)/shard_map/ppermute | solution.py:489
  13.2 5.6 %collective-permute-start.11 = (s16[272,128]{1,0:T(8,128)(2,1)S(1)}, s16[272,128]{1,0:T(8,128)(2,1)S(1)}, u32[]{:S(2)}, u32[]{:S(2)}) collective-permute-start(s16[272,128]{1,0:T(8,128)(2,1)S(1)} %get-tuple-element.59), channel_id=1, source_target_pairs={{0,4},{2,6},{4,0},{6,2},{1,5},{3,7},{5,1},{7,3},{8,12},{10,14},{12... | collective-permute-start | bytes 208904 | tf_op jit(solution)/shard_map/ppermute | solution.py:489
  14.2 11.6 %collective-permute-start.7 = (s16[272,128]{1,0:T(8,128)(2,1)S(1)}, s16[272,128]{1,0:T(8,128)(2,1)S(1)}, u32[]{:S(2)}, u32[]{:S(2)}) collective-permute-start(s16[272,128]{1,0:T(8,128)(2,1)S(1)} %get-tuple-element.55), channel_id=1, source_target_pairs={{0,2},{2,0},{4,6},{6,4},{1,3},{3,1},{5,7},{7,5},{8,10},{10,8},{12,... | collective-permute-start | bytes 208904 | tf_op jit(solution)/shard_map/ppermute | solution.py:489
  16.2 11.4 %collective-permute-start.8 = (s16[272,128]{1,0:T(8,128)(2,1)S(1)}, s16[272,128]{1,0:T(8,128)(2,1)S(1)}, u32[]{:S(2)}, u32[]{:S(2)}) collective-permute-start(s16[272,128]{1,0:T(8,128)(2,1)S(1)} %get-tuple-element.56), channel_id=1, source_target_pairs={{0,4},{2,6},{4,0},{6,2},{1,5},{3,7},{5,1},{7,3},{8,12},{10,14},{12... | collective-permute-start | bytes 208904 | tf_op jit(solution)/shard_map/ppermute | solution.py:489
  17.7 9.9 %collective-permute-start.9 = (s16[272,128]{1,0:T(8,128)(2,1)S(1)}, s16[272,128]{1,0:T(8,128)(2,1)S(1)}, u32[]{:S(2)}, u32[]{:S(2)}) collective-permute-start(s16[272,128]{1,0:T(8,128)(2,1)S(1)} %get-tuple-element.57), channel_id=1, source_target_pairs={{0,6},{2,4},{4,2},{6,0},{1,7},{3,5},{5,3},{7,1},{8,14},{10,12},{12... | collective-permute-start | bytes 208904 | tf_op jit(solution)/shard_map/ppermute | solution.py:489
  18.9 11.4 %collective-permute-start.17 = (s16[272,128]{1,0:T(8,128)(2,1)S(1)}, s16[272,128]{1,0:T(8,128)(2,1)S(1)}, u32[]{:S(2)}, u32[]{:S(2)}) collective-permute-start(s16[272,128]{1,0:T(8,128)(2,1)S(1)} %level_states_0.1.refs_3_), channel_id=1, source_target_pairs={{0,8},{8,16},{16,24},{1,9},{9,17},{17,25},{2,10},{10,18},{18,26},{... | collective-permute-start | bytes 208904 | tf_op jit(solution)/shard_map/ppermute | solution.py:496
  22.4 9.9 %collective-permute-start.16 = (s16[272,128]{1,0:T(8,128)(2,1)S(1)}, s16[272,128]{1,0:T(8,128)(2,1)S(1)}, u32[]{:S(2)}, u32[]{:S(2)}) collective-permute-start(s16[272,128]{1,0:T(8,128)(2,1)S(1)} %level_states_0.1.refs_3_), channel_id=1, source_target_pairs={{0,24},{1,25},{2,26},{3,27},{4,28},{5,29},{6,30},{7,31}} | collective-permute-start | bytes 208904 | tf_op jit(solution)/shard_map/ppermute | solution.py:496
  25.8 6.6 %collective-permute-start.15 = (s16[272,128]{1,0:T(8,128)(2,1)S(1)}, s16[272,128]{1,0:T(8,128)(2,1)S(1)}, u32[]{:S(2)}, u32[]{:S(2)}) collective-permute-start(s16[272,128]{1,0:T(8,128)(2,1)S(1)} %level_states_0.1.refs_3_), channel_id=1, source_target_pairs={{0,16},{8,24},{1,17},{9,25},{2,18},{10,26},{3,19},{11,27},{4,20},{... | collective-permute-start | bytes 208904 | tf_op jit(solution)/shard_map/ppermute | solution.py:496
  27.7 7.6 %collective-permute-start.14 = (s16[272,128]{1,0:T(8,128)(2,1)S(1)}, s16[272,128]{1,0:T(8,128)(2,1)S(1)}, u32[]{:S(2)}, u32[]{:S(2)}) collective-permute-start(s16[272,128]{1,0:T(8,128)(2,1)S(1)} %level_states_1.1.refs_7_), channel_id=1, source_target_pairs={{0,24},{1,25},{2,26},{3,27},{4,28},{5,29},{6,30},{7,31}} | collective-permute-start | bytes 208904 | tf_op jit(solution)/shard_map/ppermute | solution.py:496
  29.0 6.3 %collective-permute-start.13 = (s16[272,128]{1,0:T(8,128)(2,1)S(1)}, s16[272,128]{1,0:T(8,128)(2,1)S(1)}, u32[]{:S(2)}, u32[]{:S(2)}) collective-permute-start(s16[272,128]{1,0:T(8,128)(2,1)S(1)} %level_states_1.1.refs_7_), channel_id=1, source_target_pairs={{0,16},{8,24},{1,17},{9,25},{2,18},{10,26},{3,19},{11,27},{4,20},{... | collective-permute-start | bytes 208904 | tf_op jit(solution)/shard_map/ppermute | solution.py:496
  30.4 5.0 %collective-permute-start.12 = (s16[272,128]{1,0:T(8,128)(2,1)S(1)}, s16[272,128]{1,0:T(8,128)(2,1)S(1)}, u32[]{:S(2)}, u32[]{:S(2)}) collective-permute-start(s16[272,128]{1,0:T(8,128)(2,1)S(1)} %level_states_1.1.refs_7_), channel_id=1, source_target_pairs={{0,8},{8,16},{16,24},{1,9},{9,17},{17,25},{2,10},{10,18},{18,26},{... | collective-permute-start | bytes 208904 | tf_op jit(solution)/shard_map/ppermute | solution.py:496
  32.6 5.3 %collective-permute-start.21 = (s16[272,128]{1,0:T(8,128)(2,1)S(1)}, s16[272,128]{1,0:T(8,128)(2,1)S(1)}, u32[]{:S(2)}, u32[]{:S(2)}) collective-permute-start(s16[272,128]{1,0:T(8,128)(2,1)S(1)} %get-tuple-element.65), channel_id=1, source_target_pairs={{0,6},{2,4},{4,2},{6,0},{1,7},{3,5},{5,3},{7,1},{8,14},{10,12},{12... | collective-permute-start | bytes 208904 | tf_op jit(solution)/shard_map/ppermute | solution.py:489
  34.4 4.6 %collective-permute-start.20 = (s16[272,128]{1,0:T(8,128)(2,1)S(1)}, s16[272,128]{1,0:T(8,128)(2,1)S(1)}, u32[]{:S(2)}, u32[]{:S(2)}) collective-permute-start(s16[272,128]{1,0:T(8,128)(2,1)S(1)} %get-tuple-element.60.refs_7_), channel_id=1, source_target_pairs={{0,2},{2,0},{4,6},{6,4},{1,3},{3,1},{5,7},{7,5},{8,10},{10,8},{12,... | collective-permute-start | bytes 208904 | tf_op jit(solution)/shard_map/ppermute | solution.py:489
  35.6 6.0 %collective-permute-start.19 = (s16[272,128]{1,0:T(8,128)(2,1)S(1)}, s16[272,128]{1,0:T(8,128)(2,1)S(1)}, u32[]{:S(2)}, u32[]{:S(2)}) collective-permute-start(s16[272,128]{1,0:T(8,128)(2,1)S(1)} %get-tuple-element.62), channel_id=1, source_target_pairs={{0,6},{2,4},{4,2},{6,0},{1,7},{3,5},{5,3},{7,1},{8,14},{10,12},{12... | collective-permute-start | bytes 208904 | tf_op jit(solution)/shard_map/ppermute | solution.py:489
  37.4 5.1 %collective-permute-start.18 = (s16[272,128]{1,0:T(8,128)(2,1)S(1)}, s16[272,128]{1,0:T(8,128)(2,1)S(1)}, u32[]{:S(2)}, u32[]{:S(2)}) collective-permute-start(s16[272,128]{1,0:T(8,128)(2,1)S(1)} %get-tuple-element.61.refs_10_), channel_id=1, source_target_pairs={{0,2},{2,0},{4,6},{6,4},{1,3},{3,1},{5,7},{7,5},{8,10},{10,8},{12,... | collective-permute-start | bytes 208904 | tf_op jit(solution)/shard_map/ppermute | solution.py:489
  40.3 16.5 %collective-permute-start.24 = (bf16[512,512]{1,0:T(8,128)(2,1)S(1)}, bf16[512,512]{1,0:T(8,128)(2,1)S(1)}, u32[]{:S(2)}, u32[]{:S(2)}) collective-permute-start(bf16[512,512]{1,0:T(8,128)(2,1)S(1)} %attend_0_1_3.1.refs_10_), channel_id=1, source_target_pairs={{0,2},{2,0},{1,3},{3,1},{4,6},{6,4},{5,7},{7,5},{8,10},{10,8},{9,1... | collective-permute-start | bytes 1572872 | tf_op jit(solution)/shard_map/ppermute | solution.py:489
  43.9 19.2 %collective-permute-start.22 = (bf16[512,512]{1,0:T(8,128)(2,1)S(1)}, bf16[512,512]{1,0:T(8,128)(2,1)S(1)}, u32[]{:S(2)}, u32[]{:S(2)}) collective-permute-start(bf16[512,512]{1,0:T(8,128)(2,1)S(1)} %attend_1_1_3.1.refs_14_.refs_10_), channel_id=1, source_target_pairs={{0,2},{2,0},{1,3},{3,1},{4,6},{6,4},{5,7},{7,5},{8,10},{10,8},{9,1... | collective-permute-start | bytes 1572872 | tf_op jit(solution)/shard_map/ppermute | solution.py:489
  45.5 10.5 %collective-permute-start.25 = (f32[2,2,128,128]{3,2,1,0:T(8,128)S(1)}, f32[2,2,128,128]{3,2,1,0:T(8,128)S(1)}, u32[]{:S(2)}, u32[]{:S(2)}) collective-permute-start(f32[2,2,128,128]{3,2,1,0:T(8,128)S(1)} %get-tuple-element.69), channel_id=1, source_target_pairs={{0,4},{4,0},{1,5},{5,1},{2,6},{6,2},{3,7},{7,3},{8,12},{12,8},{9,1... | collective-permute-start | bytes 786440 | tf_op jit(solution)/shard_map/ppermute | solution.py:489
  46.9 6.5 %collective-permute-start.23 = (s16[528,128]{1,0:T(8,128)(2,1)S(1)}, s16[528,128]{1,0:T(8,128)(2,1)S(1)}, u32[]{:S(2)}, u32[]{:S(2)}) collective-permute-start(s16[528,128]{1,0:T(8,128)(2,1)S(1)} %get-tuple-element.67), channel_id=1, source_target_pairs={{0,4},{2,6},{4,0},{6,2},{1,5},{3,7},{5,1},{7,3},{8,12},{10,14},{12... | collective-permute-start | bytes 405512 | tf_op jit(solution)/shard_map/ppermute | solution.py:489

commit v19 on v16

--- a/solution.py
+++ b/solution.py
@@ -555,8 +555,7 @@
     for half in halves:
         level = level_states(plan, own[half], others[half][::-1], half, after)
         distances = [*range(1, plan.n_outer)]
-        if half == 0:
-            distances = [*distances[1:], *distances[:1]]
+        distances = [*distances[1:], *distances[:1]]
         levels.append([to_later(level, d) for d in distances])
         after = [level]
     carry = []

time: 63.5 us -> 63.5 us (level)
  no operation moved by 1% of the time
where the time goes in v19:
time: 63.5 us; the launch traced here: 63.2 us
  starting transfers between devices  33.7 us (53%)
  Pallas kernels  15.1 us (24%)
  waiting for transfers between devices  13.6 us (21%)
  between operations  0.85 us (1%)
    ppermute x20, starting transfers between devices, swap(): return lax.ppermute(array, axes, [(i, i ^ offset) for i in range(size)])  20.5 us
    ppermute x20, waiting for transfers between devices, swap(): return lax.ppermute(array, axes, [(i, i ^ offset) for i in range(size)])  13.6 us
    ppermute x6, starting transfers between devices, to_later(): return lax.ppermute(array, 'outer', pairs)  13.2 us
    pallas_call x4, Pallas kernels, attend(): pl.pallas_call(at_place(kernel), out_shape=jax.ShapeDtypeStruct((CORES *...  5.29 us
    pallas_call x1, Pallas kernels, decode(): pl.pallas_call(kernel, out_shape=[jax.ShapeDtypeStruct((rows, plan.n_y *...  3.88 us
    pallas_call x2, Pallas kernels, assemble(): pl.pallas_call(at_place(kernel), out_shape=jax.ShapeDtypeStruct((plan.n_y...  1.99 us
    pallas_call x2, Pallas kernels, chunk_states(): pl.pallas_call(at_place(kernel), out_shape=[states_shape(plan.each), stat...  1.64 us
  transfers between devices with their start and end apart: 26, of which 6 were waited for; matrix products, arithmetic and copies ran while one was open for 0% of the time, Pallas kernels for 17%

profile of v19, /device:TPU:0, one launch (start us, length us, event | category | flops | bytes accessed | tf_op | source)
XLA Modules:
  0.0 63.2 jit_solution(17994074951151457445)
XLA Ops:
  0.6 3.9 %decode.1 = (bf16[256,1024]{1,0:T(8,128)(2,1)S(1)}, bf16[256,1024]{1,0:T(8,128)(2,1)S(1)}, bf16[256,1024]{1,0:T(8,128)(2,1)S(1)}, bf16[256,1024]{1,0:T(8,128)(2,...) custom-call(s32[256,4096]{1,0:T(8,128)} %refs_0_.2, ...), custom_call_target="tpu_custom_call" | custom-call | flops 4194304 | bytes 14680064 | tf_op jit(solution)/shard_map/decode/pallas_call | solution.py:114
  4.5 0.5 collective-permute-start.3
  5.1 0.1 collective-permute-start.4
  5.1 0.3 spike_queries.1
  5.4 0.5 collective-permute-start
  5.9 0.1 collective-permute-start.5
  6.0 0.4 collective-permute-start.1
  6.4 0.2 collective-permute-done.3.refs_1_.refs_3_
  6.6 0.4 collective-permute-start.2
  7.0 0.4 collective-permute-done.4.refs_3_.refs_5_
  7.3 0.8 %chunk_states_0.1 = (f32[2,128,128]{2,1,0:T(8,128)S(1)}, f32[4,2,128,128]{3,2,1,0:T(8,128)S(1)}, s16[288,128]{1,0:T(8,128)(2,1)S(1)}, s16[272,128]{1,0:T(8,128)(2,1)S(1)}, s16[272,128]{1,0:T(8,128)(2,1)S(1)}) custom-call(bf16[256,1024]{1,0:T(8,128)(2,1)S(1)} %get-tuple-element.46.refs_0_.refs_2_, ...), custom_call_target="tpu_custom_call" | custom-call | flops 134217728 | bytes 2883584 | tf_op jit(solution)/shard_map/chunk_states_0/pallas_call | solution.py:251
  8.2 3.0 %collective-permute-start.6 = (s16[288,128]{1,0:T(8,128)(2,1)S(1)}, s16[288,128]{1,0:T(8,128)(2,1)S(1)}, u32[]{:S(2)}, u32[]{:S(2)}) collective-permute-start(s16[288,128]{1,0:T(8,128)(2,1)S(1)} %get-tuple-element.54), channel_id=1, source_target_pairs={{0,2},{2,0},{4,6},{6,4},{1,3},{3,1},{5,7},{7,5},{8,10},{10,8},{12,... | collective-permute-start | bytes 221192 | tf_op jit(solution)/shard_map/ppermute | solution.py:489
  11.1 0.0 collective-permute-done.refs_6_.refs_5_.refs_1_
  11.1 1.4 %collective-permute-start.10 = (s16[272,128]{1,0:T(8,128)(2,1)S(1)}, s16[272,128]{1,0:T(8,128)(2,1)S(1)}, u32[]{:S(2)}, u32[]{:S(2)}) collective-permute-start(s16[272,128]{1,0:T(8,128)(2,1)S(1)} %get-tuple-element.59), channel_id=1, source_target_pairs={{0,6},{2,4},{4,2},{6,0},{1,7},{3,5},{5,3},{7,1},{8,14},{10,12},{12... | collective-permute-start | bytes 208904 | tf_op jit(solution)/shard_map/ppermute | solution.py:489
  12.6 0.0 collective-permute-done.5.refs_5_.refs_4_.refs_1_
  12.6 0.1 collective-permute-start.11
  12.7 0.0 collective-permute-done.1.refs_1_.refs_3_
  12.7 0.0 collective-permute-done.2.refs_3_.refs_5_
  12.7 0.8 %chunk_states_1.1 = (f32[2,128,128]{2,1,0:T(8,128)S(1)}, f32[4,2,128,128]{3,2,1,0:T(8,128)S(1)}, s16[272,128]{1,0:T(8,128)(2,1)S(1)}, s16[272,128]{1,0:T(8,128)(2,1)S(1)}, s16[272,128]{1,0:T(8,128)(2,1)S(1)}) custom-call(bf16[256,1024]{1,0:T(8,128)(2,1)S(1)} %get-tuple-element.42.refs_0_.refs_2_, ...), custom_call_target="tpu_custom_call" | custom-call | flops 134217728 | bytes 2883584 | tf_op jit(solution)/shard_map/chunk_states_1/pallas_call | solution.py:251
  13.5 2.0 %collective-permute-start.7 = (s16[272,128]{1,0:T(8,128)(2,1)S(1)}, s16[272,128]{1,0:T(8,128)(2,1)S(1)}, u32[]{:S(2)}, u32[]{:S(2)}) collective-permute-start(s16[272,128]{1,0:T(8,128)(2,1)S(1)} %get-tuple-element.56), channel_id=1, source_target_pairs={{0,2},{2,0},{4,6},{6,4},{1,3},{3,1},{5,7},{7,5},{8,10},{10,8},{12,... | collective-permute-start | bytes 208904 | tf_op jit(solution)/shard_map/ppermute | solution.py:489
  15.5 1.5 %collective-permute-start.8 = (s16[272,128]{1,0:T(8,128)(2,1)S(1)}, s16[272,128]{1,0:T(8,128)(2,1)S(1)}, u32[]{:S(2)}, u32[]{:S(2)}) collective-permute-start(s16[272,128]{1,0:T(8,128)(2,1)S(1)} %get-tuple-element.57), channel_id=1, source_target_pairs={{0,4},{2,6},{4,0},{6,2},{1,5},{3,7},{5,1},{7,3},{8,12},{10,14},{12... | collective-permute-start | bytes 208904 | tf_op jit(solution)/shard_map/ppermute | solution.py:489
  17.0 0.0 collective-permute-done.10.refs_0_.refs_3_
  17.0 1.1 %collective-permute-start.9 = (s16[272,128]{1,0:T(8,128)(2,1)S(1)}, s16[272,128]{1,0:T(8,128)(2,1)S(1)}, u32[]{:S(2)}, u32[]{:S(2)}) collective-permute-start(s16[272,128]{1,0:T(8,128)(2,1)S(1)} %get-tuple-element.58), channel_id=1, source_target_pairs={{0,6},{2,4},{4,2},{6,0},{1,7},{3,5},{5,3},{7,1},{8,14},{10,12},{12... | collective-permute-start | bytes 208904 | tf_op jit(solution)/shard_map/ppermute | solution.py:489
  18.1 0.0 collective-permute-done.11.refs_1_.refs_2_
  18.1 0.0 collective-permute-done.6.refs_2_.refs_1_.refs_7_
  18.1 0.1 level_states_0.1.refs_3_
  18.3 3.5 %collective-permute-start.17 = (s16[272,128]{1,0:T(8,128)(2,1)S(1)}, s16[272,128]{1,0:T(8,128)(2,1)S(1)}, u32[]{:S(2)}, u32[]{:S(2)}) collective-permute-start(s16[272,128]{1,0:T(8,128)(2,1)S(1)} %level_states_0.1.refs_3_), channel_id=1, source_target_pairs={{0,8},{8,16},{16,24},{1,9},{9,17},{17,25},{2,10},{10,18},{18,26},{... | collective-permute-start | bytes 208904 | tf_op jit(solution)/shard_map/ppermute | solution.py:496
  21.7 3.3 %collective-permute-start.16 = (s16[272,128]{1,0:T(8,128)(2,1)S(1)}, s16[272,128]{1,0:T(8,128)(2,1)S(1)}, u32[]{:S(2)}, u32[]{:S(2)}) collective-permute-start(s16[272,128]{1,0:T(8,128)(2,1)S(1)} %level_states_0.1.refs_3_), channel_id=1, source_target_pairs={{0,24},{1,25},{2,26},{3,27},{4,28},{5,29},{6,30},{7,31}} | collective-permute-start | bytes 208904 | tf_op jit(solution)/shard_map/ppermute | solution.py:496
  25.1 0.0 collective-permute-done.7.refs_2_.refs_1_.refs_8_
  25.1 1.8 %collective-permute-start.15 = (s16[272,128]{1,0:T(8,128)(2,1)S(1)}, s16[272,128]{1,0:T(8,128)(2,1)S(1)}, u32[]{:S(2)}, u32[]{:S(2)}) collective-permute-start(s16[272,128]{1,0:T(8,128)(2,1)S(1)} %level_states_0.1.refs_3_), channel_id=1, source_target_pairs={{0,16},{8,24},{1,17},{9,25},{2,18},{10,26},{3,19},{11,27},{4,20},{... | collective-permute-start | bytes 208904 | tf_op jit(solution)/shard_map/ppermute | solution.py:496
  26.9 0.0 collective-permute-done.8.refs_1_.refs_2_.refs_9_
  26.9 0.0 collective-permute-done.9.refs_0_.refs_3_.refs_10_
  27.0 0.1 level_states_1.1.refs_7_
  27.1 1.9 %collective-permute-start.14 = (s16[272,128]{1,0:T(8,128)(2,1)S(1)}, s16[272,128]{1,0:T(8,128)(2,1)S(1)}, u32[]{:S(2)}, u32[]{:S(2)}) collective-permute-start(s16[272,128]{1,0:T(8,128)(2,1)S(1)} %level_states_1.1.refs_7_), channel_id=1, source_target_pairs={{0,8},{8,16},{16,24},{1,9},{9,17},{17,25},{2,10},{10,18},{18,26},{... | collective-permute-start | bytes 208904 | tf_op jit(solution)/shard_map/ppermute | solution.py:496
  29.0 1.3 %collective-permute-start.13 = (s16[272,128]{1,0:T(8,128)(2,1)S(1)}, s16[272,128]{1,0:T(8,128)(2,1)S(1)}, u32[]{:S(2)}, u32[]{:S(2)}) collective-permute-start(s16[272,128]{1,0:T(8,128)(2,1)S(1)} %level_states_1.1.refs_7_), channel_id=1, source_target_pairs={{0,24},{1,25},{2,26},{3,27},{4,28},{5,29},{6,30},{7,31}} | collective-permute-start | bytes 208904 | tf_op jit(solution)/shard_map/ppermute | solution.py:496
  30.3 0.0 collective-permute-done.17.refs_6_
  30.3 1.3 %collective-permute-start.12 = (s16[272,128]{1,0:T(8,128)(2,1)S(1)}, s16[272,128]{1,0:T(8,128)(2,1)S(1)}, u32[]{:S(2)}, u32[]{:S(2)}) collective-permute-start(s16[272,128]{1,0:T(8,128)(2,1)S(1)} %level_states_1.1.refs_7_), channel_id=1, source_target_pairs={{0,16},{8,24},{1,17},{9,25},{2,18},{10,26},{3,19},{11,27},{4,20},{... | collective-permute-start | bytes 208904 | tf_op jit(solution)/shard_map/ppermute | solution.py:496
  31.6 0.0 collective-permute-done.16.refs_5_
  31.6 0.0 collective-permute-done.15.refs_4_
  31.6 0.2 carries_0.1
  31.8 1.9 %collective-permute-start.21 = (s16[272,128]{1,0:T(8,128)(2,1)S(1)}, s16[272,128]{1,0:T(8,128)(2,1)S(1)}, u32[]{:S(2)}, u32[]{:S(2)}) collective-permute-start(s16[272,128]{1,0:T(8,128)(2,1)S(1)} %get-tuple-element.65), channel_id=1, source_target_pairs={{0,6},{2,4},{4,2},{6,0},{1,7},{3,5},{5,3},{7,1},{8,14},{10,12},{12... | collective-permute-start | bytes 208904 | tf_op jit(solution)/shard_map/ppermute | solution.py:489
  33.7 0.5 collective-permute-start.20
  34.2 0.0 collective-permute-done.14.refs_6_.refs_13_
  34.2 0.2 carries_1.1
  34.4 2.3 %collective-permute-start.19 = (s16[272,128]{1,0:T(8,128)(2,1)S(1)}, s16[272,128]{1,0:T(8,128)(2,1)S(1)}, u32[]{:S(2)}, u32[]{:S(2)}) collective-permute-start(s16[272,128]{1,0:T(8,128)(2,1)S(1)} %get-tuple-element.63), channel_id=1, source_target_pairs={{0,6},{2,4},{4,2},{6,0},{1,7},{3,5},{5,3},{7,1},{8,14},{10,12},{12... | collective-permute-start | bytes 208904 | tf_op jit(solution)/shard_map/ppermute | solution.py:489
  36.7 0.4 collective-permute-start.18
  37.2 0.0 collective-permute-done.21.refs_9_
  37.2 1.2 %collective-permute-done.20.refs_8_ = s16[272,128]{1,0:T(8,128)(2,1)S(1)} collective-permute-done((s16[272,128]{1,0:T(8,128)(2,1)S(1)}, s16[272,128]{1,0:T(8,128)(2,1)S(1)}, u32[]{:S(2)}, u32[]{:S(2)}) %collective-permute-start.20) | collective-permute-done | bytes 69664 | tf_op jit(solution)/shard_map/ppermute | solution.py:489
  38.3 1.3 %attend_0_1_3.1.refs_10_ = bf16[512,512]{1,0:T(8,128)(2,1)S(1)} custom-call(bf16[256,1024]{1,0:T(8,128)(2,1)S(1)} %get-tuple-element.50.refs_5_.refs_0_, bf16[256,1024]{1,0:T(8,128)(2,1)S(1)} %collective-permute-done.5.refs_5_.refs_4_.refs_1_, bf16[256,1024]{1,0:T(8,128)(2,1)S(1)} %get-tuple-element.46.refs_0_.refs_2_, ...), custom_call_target="tpu_custom_call" | custom-call | flops 402653184 | bytes 2097152 | tf_op jit(solution)/shard_map/attend_0_1_3/pallas_call | solution.py:415
  39.6 1.2 %collective-permute-start.24 = (bf16[512,512]{1,0:T(8,128)(2,1)S(1)}, bf16[512,512]{1,0:T(8,128)(2,1)S(1)}, u32[]{:S(2)}, u32[]{:S(2)}) collective-permute-start(bf16[512,512]{1,0:T(8,128)(2,1)S(1)} %attend_0_1_3.1.refs_10_), channel_id=1, source_target_pairs={{0,2},{2,0},{1,3},{3,1},{4,6},{6,4},{5,7},{7,5},{8,10},{10,8},{9,1... | collective-permute-start | bytes 1572872 | tf_op jit(solution)/shard_map/ppermute | solution.py:489
  40.9 1.0 %collective-permute-done.18.refs_8_ = s16[272,128]{1,0:T(8,128)(2,1)S(1)} collective-permute-done((s16[272,128]{1,0:T(8,128)(2,1)S(1)}, s16[272,128]{1,0:T(8,128)(2,1)S(1)}, u32[]{:S(2)}, u32[]{:S(2)}) %collective-permute-start.18) | collective-permute-done | bytes 69664 | tf_op jit(solution)/shard_map/ppermute | solution.py:489
  41.9 1.3 %attend_1_1_3.1.refs_14_.refs_10_ = bf16[512,512]{1,0:T(8,128)(2,1)S(1)} custom-call(bf16[256,1024]{1,0:T(8,128)(2,1)S(1)} %get-tuple-element.40.refs_0_, bf16[256,1024]{1,0:T(8,128)(2,1)S(1)} %collective-permute-done.refs_6_.refs_5_.refs_1_, bf16[256,1024]{1,0:T(8,128)(2,1)S(1)} %get-tuple-element.42.refs_0_.refs_2_, ...), custom_call_target="tpu_custom_call" | custom-call | flops 402653184 | bytes 2097152 | tf_op jit(solution)/shard_map/attend_1_1_3/pallas_call | solution.py:415
  43.2 1.0 %collective-permute-start.22 = (bf16[512,512]{1,0:T(8,128)(2,1)S(1)}, bf16[512,512]{1,0:T(8,128)(2,1)S(1)}, u32[]{:S(2)}, u32[]{:S(2)}) collective-permute-start(bf16[512,512]{1,0:T(8,128)(2,1)S(1)} %attend_1_1_3.1.refs_14_.refs_10_), channel_id=1, source_target_pairs={{0,2},{2,0},{1,3},{3,1},{4,6},{6,4},{5,7},{7,5},{8,10},{10,8},{9,1... | collective-permute-start | bytes 1572872 | tf_op jit(solution)/shard_map/ppermute | solution.py:489
  44.2 0.6 own_carries.1
  44.8 1.0 %collective-permute-start.25 = (f32[2,2,128,128]{3,2,1,0:T(8,128)S(1)}, f32[2,2,128,128]{3,2,1,0:T(8,128)S(1)}, u32[]{:S(2)}, u32[]{:S(2)}) collective-permute-start(f32[2,2,128,128]{3,2,1,0:T(8,128)S(1)} %get-tuple-element.69), channel_id=1, source_target_pairs={{0,4},{4,0},{1,5},{5,1},{2,6},{6,2},{3,7},{7,3},{8,12},{12,8},{9,1... | collective-permute-start | bytes 786440 | tf_op jit(solution)/shard_map/ppermute | solution.py:489
  45.8 1.1 %collective-permute-start.23 = (s16[528,128]{1,0:T(8,128)(2,1)S(1)}, s16[528,128]{1,0:T(8,128)(2,1)S(1)}, u32[]{:S(2)}, u32[]{:S(2)}) collective-permute-start(s16[528,128]{1,0:T(8,128)(2,1)S(1)} %get-tuple-element.67), channel_id=1, source_target_pairs={{0,4},{2,6},{4,0},{6,2},{1,5},{3,7},{5,1},{7,3},{8,12},{10,14},{12... | collective-permute-start | bytes 405512 | tf_op jit(solution)/shard_map/ppermute | solution.py:489
  46.9 5.8 %collective-permute-done.23.refs_9_ = s16[528,128]{1,0:T(8,128)(2,1)S(1)} collective-permute-done((s16[528,128]{1,0:T(8,128)(2,1)S(1)}, s16[528,128]{1,0:T(8,128)(2,1)S(1)}, u32[]{:S(2)}, u32[]{:S(2)}) %collective-permute-start.23) | collective-permute-done | bytes 135200 | tf_op jit(solution)/shard_map/ppermute | solution.py:489
  52.7 1.3 %attend_0_0_2.1.refs_10_.refs_0_ = bf16[512,512]{1,0:T(8,128)(2,1)S(1)} custom-call(bf16[256,1024]{1,0:T(8,128)(2,1)S(1)} %get-tuple-element.50.refs_5_.refs_0_, bf16[256,1024]{1,0:T(8,128)(2,1)S(1)} %collective-permute-done.5.refs_5_.refs_4_.refs_1_, bf16[256,1024]{1,0:T(8,128)(2,1)S(1)} %get-tuple-element.46.refs_0_.refs_2_, ...), custom_call_target="tpu_custom_call" | custom-call | flops 402653184 | bytes 2097152 | tf_op jit(solution)/shard_map/attend_0_0_2/pallas_call | solution.py:415
  54.0 1.3 %attend_1_0_2.1.refs_1_ = bf16[512,512]{1,0:T(8,128)(2,1)S(1)} custom-call(bf16[256,1024]{1,0:T(8,128)(2,1)S(1)} %get-tuple-element.40.refs_0_, bf16[256,1024]{1,0:T(8,128)(2,1)S(1)} %collective-permute-done.refs_6_.refs_5_.refs_1_, bf16[256,1024]{1,0:T(8,128)(2,1)S(1)} %get-tuple-element.42.refs_0_.refs_2_, ...), custom_call_target="tpu_custom_call" | custom-call | flops 402653184 | bytes 2097152 | tf_op jit(solution)/shard_map/attend_1_0_2/pallas_call | solution.py:415
  55.4 0.8 %assemble_cache.1 = f32[1,8,128,128]{3,2,1,0:T(8,128)} custom-call(f32[2,2,128,128]{3,2,1,0:T(8,128)S(1)} %get-tuple-element.68.refs_0_, f32[2,2,128,128]{3,2,1,0:T(8,128)S(1)} %collective-permute-done.25.refs_1_), custom_call_target="tpu_custom_call" | custom-call | tf_op jit(solution)/shard_map/assemble_cache/pallas_call | solution.py:475
  56.2 0.0 collective-permute-done.24.refs_2_
  56.2 1.2 %assemble.1.refs_1_ = bf16[1024,1024]{1,0:T(8,128)(2,1)} custom-call(bf16[512,512]{1,0:T(8,128)(2,1)S(1)} %attend_0_0_2.1.refs_10_.refs_0_, bf16[512,512]{1,0:T(8,128)(2,1)S(1)} %attend_1_0_2.1.refs_1_, bf16[512,512]{1,0:T(8,128)(2,1)S(1)} %collective-permute-done.24.refs_2_), custom_call_target="tpu_custom_call" | custom-call | tf_op jit(solution)/shard_map/assemble/pallas_call | solution.py:454
  57.4 5.0 %collective-permute-done.22.refs_0_ = bf16[512,512]{1,0:T(8,128)(2,1)S(1)} collective-permute-done((bf16[512,512]{1,0:T(8,128)(2,1)S(1)}, bf16[512,512]{1,0:T(8,128)(2,1)S(1)}, u32[]{:S(2)}, u32[]{:S(2)}) %collective-permute-start.22) | collective-permute-done | bytes 524320 | tf_op jit(solution)/shard_map/ppermute | solution.py:489
  62.4 0.8 %finish.1 = bf16[1024,1024]{1,0:T(8,128)(2,1)} custom-call(bf16[512,512]{1,0:T(8,128)(2,1)S(1)} %collective-permute-done.22.refs_0_, bf16[1024,1024]{1,0:T(8,128)(2,1)} %assemble.1.refs_1_), custom_call_target="tpu_custom_call", output_to_operand_aliasing={{}: (1, {})} | custom-call | tf_op jit(solution)/shard_map/finish/pallas_call | solution.py:454
  (8 shorter events, 0.0 us)
Async XLA Ops:
  0.6 4.5 %copy-start = (bf16[256,4096]{1,0:T(8,128)(2,1)S(1)}, bf16[256,4096]{1,0:T(8,128)(2,1)}, u32[]{:S(2)}) copy-start(bf16[256,4096]{1,0:T(8,128)(2,1)} %refs_0_.3) | copy-start | bytes 6291460
  4.5 2.1 %collective-permute-start.3 = (bf16[256,1024]{1,0:T(8,128)(2,1)S(1)}, bf16[256,1024]{1,0:T(8,128)(2,1)S(1)}, u32[]{:S(2)}, u32[]{:S(2)}) collective-permute-start(bf16[256,1024]{1,0:T(8,128)(2,1)S(1)} %get-tuple-element.47), channel_id=1, source_target_pairs={{0,1},{1,0},{2,3},{3,2},{4,5},{5,4},{6,7},{7,6},{8,9},{9,8},{10,11... | collective-permute-start | bytes 1572872 | tf_op jit(solution)/shard_map/ppermute | solution.py:489
  5.1 2.3 %collective-permute-start.4 = (bf16[256,1024]{1,0:T(8,128)(2,1)S(1)}, bf16[256,1024]{1,0:T(8,128)(2,1)S(1)}, u32[]{:S(2)}, u32[]{:S(2)}) collective-permute-start(bf16[256,1024]{1,0:T(8,128)(2,1)S(1)} %get-tuple-element.49), channel_id=1, source_target_pairs={{0,1},{1,0},{2,3},{3,2},{4,5},{5,4},{6,7},{7,6},{8,9},{9,8},{10,11... | collective-permute-start | bytes 1572872 | tf_op jit(solution)/shard_map/ppermute | solution.py:489
  5.1 2.2 %copy-start.1 = (f32[1024]{0:T(1024)S(1)}, f32[1024]{0:T(1024)}, u32[]{:S(2)}) copy-start(f32[1024]{0:T(1024)} %param.9) | copy-start | bytes 12292
  5.4 5.7 %collective-permute-start = (bf16[256,1024]{1,0:T(8,128)(2,1)S(1)}, bf16[256,1024]{1,0:T(8,128)(2,1)S(1)}, u32[]{:S(2)}, u32[]{:S(2)}) collective-permute-start(bf16[256,1024]{1,0:T(8,128)(2,1)S(1)} %get-tuple-element.41), channel_id=1, source_target_pairs={{0,1},{1,0},{2,3},{3,2},{4,5},{5,4},{6,7},{7,6},{8,9},{9,8},{10,11... | collective-permute-start | bytes 1572872 | tf_op jit(solution)/shard_map/ppermute | solution.py:489
  5.9 6.6 %collective-permute-start.5 = (bf16[256,1024]{1,0:T(8,128)(2,1)S(1)}, bf16[256,1024]{1,0:T(8,128)(2,1)S(1)}, u32[]{:S(2)}, u32[]{:S(2)}) collective-permute-start(bf16[256,1024]{1,0:T(8,128)(2,1)S(1)} %get-tuple-element.52), channel_id=1, source_target_pairs={{0,1},{1,0},{2,3},{3,2},{4,5},{5,4},{6,7},{7,6},{8,9},{9,8},{10,11... | collective-permute-start | bytes 1572872 | tf_op jit(solution)/shard_map/ppermute | solution.py:489
  6.0 6.7 %collective-permute-start.1 = (bf16[256,1024]{1,0:T(8,128)(2,1)S(1)}, bf16[256,1024]{1,0:T(8,128)(2,1)S(1)}, u32[]{:S(2)}, u32[]{:S(2)}) collective-permute-start(bf16[256,1024]{1,0:T(8,128)(2,1)S(1)} %get-tuple-element.43), channel_id=1, source_target_pairs={{0,1},{1,0},{2,3},{3,2},{4,5},{5,4},{6,7},{7,6},{8,9},{9,8},{10,11... | collective-permute-start | bytes 1572872 | tf_op jit(solution)/shard_map/ppermute | solution.py:489
  6.6 6.1 %collective-permute-start.2 = (bf16[256,1024]{1,0:T(8,128)(2,1)S(1)}, bf16[256,1024]{1,0:T(8,128)(2,1)S(1)}, u32[]{:S(2)}, u32[]{:S(2)}) collective-permute-start(bf16[256,1024]{1,0:T(8,128)(2,1)S(1)} %get-tuple-element.45), channel_id=1, source_target_pairs={{0,1},{1,0},{2,3},{3,2},{4,5},{5,4},{6,7},{7,6},{8,9},{9,8},{10,11... | collective-permute-start | bytes 1572872 | tf_op jit(solution)/shard_map/ppermute | solution.py:489
  8.2 10.0 %collective-permute-start.6 = (s16[288,128]{1,0:T(8,128)(2,1)S(1)}, s16[288,128]{1,0:T(8,128)(2,1)S(1)}, u32[]{:S(2)}, u32[]{:S(2)}) collective-permute-start(s16[288,128]{1,0:T(8,128)(2,1)S(1)} %get-tuple-element.54), channel_id=1, source_target_pairs={{0,2},{2,0},{4,6},{6,4},{1,3},{3,1},{5,7},{7,5},{8,10},{10,8},{12,... | collective-permute-start | bytes 221192 | tf_op jit(solution)/shard_map/ppermute | solution.py:489
  11.1 5.9 %collective-permute-start.10 = (s16[272,128]{1,0:T(8,128)(2,1)S(1)}, s16[272,128]{1,0:T(8,128)(2,1)S(1)}, u32[]{:S(2)}, u32[]{:S(2)}) collective-permute-start(s16[272,128]{1,0:T(8,128)(2,1)S(1)} %get-tuple-element.59), channel_id=1, source_target_pairs={{0,6},{2,4},{4,2},{6,0},{1,7},{3,5},{5,3},{7,1},{8,14},{10,12},{12... | collective-permute-start | bytes 208904 | tf_op jit(solution)/shard_map/ppermute | solution.py:489
  12.6 5.6 %collective-permute-start.11 = (s16[272,128]{1,0:T(8,128)(2,1)S(1)}, s16[272,128]{1,0:T(8,128)(2,1)S(1)}, u32[]{:S(2)}, u32[]{:S(2)}) collective-permute-start(s16[272,128]{1,0:T(8,128)(2,1)S(1)} %get-tuple-element.60), channel_id=1, source_target_pairs={{0,4},{2,6},{4,0},{6,2},{1,5},{3,7},{5,1},{7,3},{8,12},{10,14},{12... | collective-permute-start | bytes 208904 | tf_op jit(solution)/shard_map/ppermute | solution.py:489
  13.5 11.6 %collective-permute-start.7 = (s16[272,128]{1,0:T(8,128)(2,1)S(1)}, s16[272,128]{1,0:T(8,128)(2,1)S(1)}, u32[]{:S(2)}, u32[]{:S(2)}) collective-permute-start(s16[272,128]{1,0:T(8,128)(2,1)S(1)} %get-tuple-element.56), channel_id=1, source_target_pairs={{0,2},{2,0},{4,6},{6,4},{1,3},{3,1},{5,7},{7,5},{8,10},{10,8},{12,... | collective-permute-start | bytes 208904 | tf_op jit(solution)/shard_map/ppermute | solution.py:489
  15.5 11.4 %collective-permute-start.8 = (s16[272,128]{1,0:T(8,128)(2,1)S(1)}, s16[272,128]{1,0:T(8,128)(2,1)S(1)}, u32[]{:S(2)}, u32[]{:S(2)}) collective-permute-start(s16[272,128]{1,0:T(8,128)(2,1)S(1)} %get-tuple-element.57), channel_id=1, source_target_pairs={{0,4},{2,6},{4,0},{6,2},{1,5},{3,7},{5,1},{7,3},{8,12},{10,14},{12... | collective-permute-start | bytes 208904 | tf_op jit(solution)/shard_map/ppermute | solution.py:489
  17.0 9.9 %collective-permute-start.9 = (s16[272,128]{1,0:T(8,128)(2,1)S(1)}, s16[272,128]{1,0:T(8,128)(2,1)S(1)}, u32[]{:S(2)}, u32[]{:S(2)}) collective-permute-start(s16[272,128]{1,0:T(8,128)(2,1)S(1)} %get-tuple-element.58), channel_id=1, source_target_pairs={{0,6},{2,4},{4,2},{6,0},{1,7},{3,5},{5,3},{7,1},{8,14},{10,12},{12... | collective-permute-start | bytes 208904 | tf_op jit(solution)/shard_map/ppermute | solution.py:489
  18.3 12.0 %collective-permute-start.17 = (s16[272,128]{1,0:T(8,128)(2,1)S(1)}, s16[272,128]{1,0:T(8,128)(2,1)S(1)}, u32[]{:S(2)}, u32[]{:S(2)}) collective-permute-start(s16[272,128]{1,0:T(8,128)(2,1)S(1)} %level_states_0.1.refs_3_), channel_id=1, source_target_pairs={{0,8},{8,16},{16,24},{1,9},{9,17},{17,25},{2,10},{10,18},{18,26},{... | collective-permute-start | bytes 208904 | tf_op jit(solution)/shard_map/ppermute | solution.py:496
  21.7 9.9 %collective-permute-start.16 = (s16[272,128]{1,0:T(8,128)(2,1)S(1)}, s16[272,128]{1,0:T(8,128)(2,1)S(1)}, u32[]{:S(2)}, u32[]{:S(2)}) collective-permute-start(s16[272,128]{1,0:T(8,128)(2,1)S(1)} %level_states_0.1.refs_3_), channel_id=1, source_target_pairs={{0,24},{1,25},{2,26},{3,27},{4,28},{5,29},{6,30},{7,31}} | collective-permute-start | bytes 208904 | tf_op jit(solution)/shard_map/ppermute | solution.py:496
  25.1 6.5 %collective-permute-start.15 = (s16[272,128]{1,0:T(8,128)(2,1)S(1)}, s16[272,128]{1,0:T(8,128)(2,1)S(1)}, u32[]{:S(2)}, u32[]{:S(2)}) collective-permute-start(s16[272,128]{1,0:T(8,128)(2,1)S(1)} %level_states_0.1.refs_3_), channel_id=1, source_target_pairs={{0,16},{8,24},{1,17},{9,25},{2,18},{10,26},{3,19},{11,27},{4,20},{... | collective-permute-start | bytes 208904 | tf_op jit(solution)/shard_map/ppermute | solution.py:496
  27.1 7.1 %collective-permute-start.14 = (s16[272,128]{1,0:T(8,128)(2,1)S(1)}, s16[272,128]{1,0:T(8,128)(2,1)S(1)}, u32[]{:S(2)}, u32[]{:S(2)}) collective-permute-start(s16[272,128]{1,0:T(8,128)(2,1)S(1)} %level_states_1.1.refs_7_), channel_id=1, source_target_pairs={{0,8},{8,16},{16,24},{1,9},{9,17},{17,25},{2,10},{10,18},{18,26},{... | collective-permute-start | bytes 208904 | tf_op jit(solution)/shard_map/ppermute | solution.py:496
  29.0 5.2 %collective-permute-start.13 = (s16[272,128]{1,0:T(8,128)(2,1)S(1)}, s16[272,128]{1,0:T(8,128)(2,1)S(1)}, u32[]{:S(2)}, u32[]{:S(2)}) collective-permute-start(s16[272,128]{1,0:T(8,128)(2,1)S(1)} %level_states_1.1.refs_7_), channel_id=1, source_target_pairs={{0,24},{1,25},{2,26},{3,27},{4,28},{5,29},{6,30},{7,31}} | collective-permute-start | bytes 208904 | tf_op jit(solution)/shard_map/ppermute | solution.py:496
  30.3 3.9 %collective-permute-start.12 = (s16[272,128]{1,0:T(8,128)(2,1)S(1)}, s16[272,128]{1,0:T(8,128)(2,1)S(1)}, u32[]{:S(2)}, u32[]{:S(2)}) collective-permute-start(s16[272,128]{1,0:T(8,128)(2,1)S(1)} %level_states_1.1.refs_7_), channel_id=1, source_target_pairs={{0,16},{8,24},{1,17},{9,25},{2,18},{10,26},{3,19},{11,27},{4,20},{... | collective-permute-start | bytes 208904 | tf_op jit(solution)/shard_map/ppermute | solution.py:496
  31.8 5.3 %collective-permute-start.21 = (s16[272,128]{1,0:T(8,128)(2,1)S(1)}, s16[272,128]{1,0:T(8,128)(2,1)S(1)}, u32[]{:S(2)}, u32[]{:S(2)}) collective-permute-start(s16[272,128]{1,0:T(8,128)(2,1)S(1)} %get-tuple-element.65), channel_id=1, source_target_pairs={{0,6},{2,4},{4,2},{6,0},{1,7},{3,5},{5,3},{7,1},{8,14},{10,12},{12... | collective-permute-start | bytes 208904 | tf_op jit(solution)/shard_map/ppermute | solution.py:489
  33.7 4.6 %collective-permute-start.20 = (s16[272,128]{1,0:T(8,128)(2,1)S(1)}, s16[272,128]{1,0:T(8,128)(2,1)S(1)}, u32[]{:S(2)}, u32[]{:S(2)}) collective-permute-start(s16[272,128]{1,0:T(8,128)(2,1)S(1)} %get-tuple-element.61.refs_7_), channel_id=1, source_target_pairs={{0,2},{2,0},{4,6},{6,4},{1,3},{3,1},{5,7},{7,5},{8,10},{10,8},{12,... | collective-permute-start | bytes 208904 | tf_op jit(solution)/shard_map/ppermute | solution.py:489
  34.4 6.4 %collective-permute-start.19 = (s16[272,128]{1,0:T(8,128)(2,1)S(1)}, s16[272,128]{1,0:T(8,128)(2,1)S(1)}, u32[]{:S(2)}, u32[]{:S(2)}) collective-permute-start(s16[272,128]{1,0:T(8,128)(2,1)S(1)} %get-tuple-element.63), channel_id=1, source_target_pairs={{0,6},{2,4},{4,2},{6,0},{1,7},{3,5},{5,3},{7,1},{8,14},{10,12},{12... | collective-permute-start | bytes 208904 | tf_op jit(solution)/shard_map/ppermute | solution.py:489
  36.7 5.1 %collective-permute-start.18 = (s16[272,128]{1,0:T(8,128)(2,1)S(1)}, s16[272,128]{1,0:T(8,128)(2,1)S(1)}, u32[]{:S(2)}, u32[]{:S(2)}) collective-permute-start(s16[272,128]{1,0:T(8,128)(2,1)S(1)} %get-tuple-element.62.refs_10_), channel_id=1, source_target_pairs={{0,2},{2,0},{4,6},{6,4},{1,3},{3,1},{5,7},{7,5},{8,10},{10,8},{12,... | collective-permute-start | bytes 208904 | tf_op jit(solution)/shard_map/ppermute | solution.py:489
  39.6 16.6 %collective-permute-start.24 = (bf16[512,512]{1,0:T(8,128)(2,1)S(1)}, bf16[512,512]{1,0:T(8,128)(2,1)S(1)}, u32[]{:S(2)}, u32[]{:S(2)}) collective-permute-start(bf16[512,512]{1,0:T(8,128)(2,1)S(1)} %attend_0_1_3.1.refs_10_), channel_id=1, source_target_pairs={{0,2},{2,0},{1,3},{3,1},{4,6},{6,4},{5,7},{7,5},{8,10},{10,8},{9,1... | collective-permute-start | bytes 1572872 | tf_op jit(solution)/shard_map/ppermute | solution.py:489
  43.2 19.2 %collective-permute-start.22 = (bf16[512,512]{1,0:T(8,128)(2,1)S(1)}, bf16[512,512]{1,0:T(8,128)(2,1)S(1)}, u32[]{:S(2)}, u32[]{:S(2)}) collective-permute-start(bf16[512,512]{1,0:T(8,128)(2,1)S(1)} %attend_1_1_3.1.refs_14_.refs_10_), channel_id=1, source_target_pairs={{0,2},{2,0},{1,3},{3,1},{4,6},{6,4},{5,7},{7,5},{8,10},{10,8},{9,1... | collective-permute-start | bytes 1572872 | tf_op jit(solution)/shard_map/ppermute | solution.py:489
  44.8 10.5 %collective-permute-start.25 = (f32[2,2,128,128]{3,2,1,0:T(8,128)S(1)}, f32[2,2,128,128]{3,2,1,0:T(8,128)S(1)}, u32[]{:S(2)}, u32[]{:S(2)}) collective-permute-start(f32[2,2,128,128]{3,2,1,0:T(8,128)S(1)} %get-tuple-element.69), channel_id=1, source_target_pairs={{0,4},{4,0},{1,5},{5,1},{2,6},{6,2},{3,7},{7,3},{8,12},{12,8},{9,1... | collective-permute-start | bytes 786440 | tf_op jit(solution)/shard_map/ppermute | solution.py:489
  45.8 6.9 %collective-permute-start.23 = (s16[528,128]{1,0:T(8,128)(2,1)S(1)}, s16[528,128]{1,0:T(8,128)(2,1)S(1)}, u32[]{:S(2)}, u32[]{:S(2)}) collective-permute-start(s16[528,128]{1,0:T(8,128)(2,1)S(1)} %get-tuple-element.67), channel_id=1, source_target_pairs={{0,4},{2,6},{4,0},{6,2},{1,5},{3,7},{5,1},{7,3},{8,12},{10,14},{12... | collective-permute-start | bytes 405512 | tf_op jit(solution)/shard_map/ppermute | solution.py:489

commit v20 on v19

--- a/solution.py
+++ b/solution.py
@@ -80,7 +80,7 @@
 
 def decode(plan, spikes, keys, values):
     rows, model = spikes.shape
-    step = min(rows, 32)
+    step = min(rows, 16)
     chunks = rows // step
     n_out = 3 * CORES * plan.halves
 

time: 63.5 us -> 63.6 us (level)
  transfers between devices with their start and end apart: 26 -> 26, of which waited for: 6 -> 6; matrix products, arithmetic and copies ran while one was open for 0% -> 0% of each run, Pallas kernels for 17% -> 16%
where the time goes in v20:
time: 63.6 us; the launch traced here: 63.4 us
  starting transfers between devices  33.7 us (53%)
  Pallas kernels  15.3 us (24%)
  waiting for transfers between devices  13.6 us (21%)
  between operations  0.85 us (1%)
    ppermute x20, starting transfers between devices, swap(): return lax.ppermute(array, axes, [(i, i ^ offset) for i in range(size)])  20.5 us
    ppermute x20, waiting for transfers between devices, swap(): return lax.ppermute(array, axes, [(i, i ^ offset) for i in range(size)])  13.6 us
    ppermute x6, starting transfers between devices, to_later(): return lax.ppermute(array, 'outer', pairs)  13.2 us
    pallas_call x4, Pallas kernels, attend(): pl.pallas_call(at_place(kernel), out_shape=jax.ShapeDtypeStruct((CORES *...  5.28 us
    pallas_call x1, Pallas kernels, decode(): pl.pallas_call(kernel, out_shape=[jax.ShapeDtypeStruct((rows, plan.n_y *...  4.05 us
    pallas_call x2, Pallas kernels, assemble(): pl.pallas_call(at_place(kernel), out_shape=jax.ShapeDtypeStruct((plan.n_y...  1.99 us
    pallas_call x2, Pallas kernels, chunk_states(): pl.pallas_call(at_place(kernel), out_shape=[states_shape(plan.each), stat...  1.64 us
  transfers between devices with their start and end apart: 26, of which 6 were waited for; matrix products, arithmetic and copies ran while one was open for 0% of the time, Pallas kernels for 16%

profile of v20, /device:TPU:0, one launch (start us, length us, event | category | flops | bytes accessed | tf_op | source)
XLA Modules:
  0.0 63.4 jit_solution(16417842186542063356)
XLA Ops:
  0.6 4.0 %decode.1 = (bf16[256,1024]{1,0:T(8,128)(2,1)S(1)}, bf16[256,1024]{1,0:T(8,128)(2,1)S(1)}, bf16[256,1024]{1,0:T(8,128)(2,1)S(1)}, bf16[256,1024]{1,0:T(8,128)(2,...) custom-call(s32[256,4096]{1,0:T(8,128)} %refs_0_.2, ...), custom_call_target="tpu_custom_call" | custom-call | flops 4194304 | bytes 14680064 | tf_op jit(solution)/shard_map/decode/pallas_call | solution.py:114
  4.7 0.5 collective-permute-start.3
  5.2 0.1 collective-permute-start.4
  5.3 0.3 spike_queries.1
  5.6 0.5 collective-permute-start
  6.1 0.1 collective-permute-start.5
  6.2 0.4 collective-permute-start.1
  6.6 0.2 collective-permute-done.3.refs_1_.refs_3_
  6.8 0.4 collective-permute-start.2
  7.1 0.4 collective-permute-done.4.refs_3_.refs_5_
  7.5 0.8 %chunk_states_0.1 = (f32[2,128,128]{2,1,0:T(8,128)S(1)}, f32[4,2,128,128]{3,2,1,0:T(8,128)S(1)}, s16[288,128]{1,0:T(8,128)(2,1)S(1)}, s16[272,128]{1,0:T(8,128)(2,1)S(1)}, s16[272,128]{1,0:T(8,128)(2,1)S(1)}) custom-call(bf16[256,1024]{1,0:T(8,128)(2,1)S(1)} %get-tuple-element.46.refs_0_.refs_2_, ...), custom_call_target="tpu_custom_call" | custom-call | flops 134217728 | bytes 2883584 | tf_op jit(solution)/shard_map/chunk_states_0/pallas_call | solution.py:251
  8.3 3.0 %collective-permute-start.6 = (s16[288,128]{1,0:T(8,128)(2,1)S(1)}, s16[288,128]{1,0:T(8,128)(2,1)S(1)}, u32[]{:S(2)}, u32[]{:S(2)}) collective-permute-start(s16[288,128]{1,0:T(8,128)(2,1)S(1)} %get-tuple-element.54), channel_id=1, source_target_pairs={{0,2},{2,0},{4,6},{6,4},{1,3},{3,1},{5,7},{7,5},{8,10},{10,8},{12,... | collective-permute-start | bytes 221192 | tf_op jit(solution)/shard_map/ppermute | solution.py:489
  11.3 1.4 %collective-permute-start.10 = (s16[272,128]{1,0:T(8,128)(2,1)S(1)}, s16[272,128]{1,0:T(8,128)(2,1)S(1)}, u32[]{:S(2)}, u32[]{:S(2)}) collective-permute-start(s16[272,128]{1,0:T(8,128)(2,1)S(1)} %get-tuple-element.59), channel_id=1, source_target_pairs={{0,6},{2,4},{4,2},{6,0},{1,7},{3,5},{5,3},{7,1},{8,14},{10,12},{12... | collective-permute-start | bytes 208904 | tf_op jit(solution)/shard_map/ppermute | solution.py:489
  12.7 0.1 collective-permute-start.11
  12.9 0.0 collective-permute-done.1.refs_1_.refs_3_
  12.9 0.0 collective-permute-done.2.refs_3_.refs_5_
  12.9 0.8 %chunk_states_1.1 = (f32[2,128,128]{2,1,0:T(8,128)S(1)}, f32[4,2,128,128]{3,2,1,0:T(8,128)S(1)}, s16[272,128]{1,0:T(8,128)(2,1)S(1)}, s16[272,128]{1,0:T(8,128)(2,1)S(1)}, s16[272,128]{1,0:T(8,128)(2,1)S(1)}) custom-call(bf16[256,1024]{1,0:T(8,128)(2,1)S(1)} %get-tuple-element.42.refs_0_.refs_2_, ...), custom_call_target="tpu_custom_call" | custom-call | flops 134217728 | bytes 2883584 | tf_op jit(solution)/shard_map/chunk_states_1/pallas_call | solution.py:251
  13.7 2.0 %collective-permute-start.7 = (s16[272,128]{1,0:T(8,128)(2,1)S(1)}, s16[272,128]{1,0:T(8,128)(2,1)S(1)}, u32[]{:S(2)}, u32[]{:S(2)}) collective-permute-start(s16[272,128]{1,0:T(8,128)(2,1)S(1)} %get-tuple-element.56), channel_id=1, source_target_pairs={{0,2},{2,0},{4,6},{6,4},{1,3},{3,1},{5,7},{7,5},{8,10},{10,8},{12,... | collective-permute-start | bytes 208904 | tf_op jit(solution)/shard_map/ppermute | solution.py:489
  15.7 1.5 %collective-permute-start.8 = (s16[272,128]{1,0:T(8,128)(2,1)S(1)}, s16[272,128]{1,0:T(8,128)(2,1)S(1)}, u32[]{:S(2)}, u32[]{:S(2)}) collective-permute-start(s16[272,128]{1,0:T(8,128)(2,1)S(1)} %get-tuple-element.57), channel_id=1, source_target_pairs={{0,4},{2,6},{4,0},{6,2},{1,5},{3,7},{5,1},{7,3},{8,12},{10,14},{12... | collective-permute-start | bytes 208904 | tf_op jit(solution)/shard_map/ppermute | solution.py:489
  17.2 0.0 collective-permute-done.10.refs_0_.refs_3_
  17.2 1.1 %collective-permute-start.9 = (s16[272,128]{1,0:T(8,128)(2,1)S(1)}, s16[272,128]{1,0:T(8,128)(2,1)S(1)}, u32[]{:S(2)}, u32[]{:S(2)}) collective-permute-start(s16[272,128]{1,0:T(8,128)(2,1)S(1)} %get-tuple-element.58), channel_id=1, source_target_pairs={{0,6},{2,4},{4,2},{6,0},{1,7},{3,5},{5,3},{7,1},{8,14},{10,12},{12... | collective-permute-start | bytes 208904 | tf_op jit(solution)/shard_map/ppermute | solution.py:489
  18.3 0.0 collective-permute-done.11.refs_1_.refs_2_
  18.3 0.0 collective-permute-done.6.refs_2_.refs_1_.refs_7_
  18.3 0.1 level_states_0.1.refs_3_
  18.4 3.5 %collective-permute-start.17 = (s16[272,128]{1,0:T(8,128)(2,1)S(1)}, s16[272,128]{1,0:T(8,128)(2,1)S(1)}, u32[]{:S(2)}, u32[]{:S(2)}) collective-permute-start(s16[272,128]{1,0:T(8,128)(2,1)S(1)} %level_states_0.1.refs_3_), channel_id=1, source_target_pairs={{0,8},{8,16},{16,24},{1,9},{9,17},{17,25},{2,10},{10,18},{18,26},{... | collective-permute-start | bytes 208904 | tf_op jit(solution)/shard_map/ppermute | solution.py:496
  21.9 3.3 %collective-permute-start.16 = (s16[272,128]{1,0:T(8,128)(2,1)S(1)}, s16[272,128]{1,0:T(8,128)(2,1)S(1)}, u32[]{:S(2)}, u32[]{:S(2)}) collective-permute-start(s16[272,128]{1,0:T(8,128)(2,1)S(1)} %level_states_0.1.refs_3_), channel_id=1, source_target_pairs={{0,24},{1,25},{2,26},{3,27},{4,28},{5,29},{6,30},{7,31}} | collective-permute-start | bytes 208904 | tf_op jit(solution)/shard_map/ppermute | solution.py:496
  25.2 0.0 collective-permute-done.7.refs_2_.refs_1_.refs_8_
  25.2 1.8 %collective-permute-start.15 = (s16[272,128]{1,0:T(8,128)(2,1)S(1)}, s16[272,128]{1,0:T(8,128)(2,1)S(1)}, u32[]{:S(2)}, u32[]{:S(2)}) collective-permute-start(s16[272,128]{1,0:T(8,128)(2,1)S(1)} %level_states_0.1.refs_3_), channel_id=1, source_target_pairs={{0,16},{8,24},{1,17},{9,25},{2,18},{10,26},{3,19},{11,27},{4,20},{... | collective-permute-start | bytes 208904 | tf_op jit(solution)/shard_map/ppermute | solution.py:496
  27.1 0.0 collective-permute-done.8.refs_1_.refs_2_.refs_9_
  27.1 0.0 collective-permute-done.9.refs_0_.refs_3_.refs_10_
  27.1 0.1 level_states_1.1.refs_7_
  27.2 1.9 %collective-permute-start.14 = (s16[272,128]{1,0:T(8,128)(2,1)S(1)}, s16[272,128]{1,0:T(8,128)(2,1)S(1)}, u32[]{:S(2)}, u32[]{:S(2)}) collective-permute-start(s16[272,128]{1,0:T(8,128)(2,1)S(1)} %level_states_1.1.refs_7_), channel_id=1, source_target_pairs={{0,8},{8,16},{16,24},{1,9},{9,17},{17,25},{2,10},{10,18},{18,26},{... | collective-permute-start | bytes 208904 | tf_op jit(solution)/shard_map/ppermute | solution.py:496
  29.2 1.3 %collective-permute-start.13 = (s16[272,128]{1,0:T(8,128)(2,1)S(1)}, s16[272,128]{1,0:T(8,128)(2,1)S(1)}, u32[]{:S(2)}, u32[]{:S(2)}) collective-permute-start(s16[272,128]{1,0:T(8,128)(2,1)S(1)} %level_states_1.1.refs_7_), channel_id=1, source_target_pairs={{0,24},{1,25},{2,26},{3,27},{4,28},{5,29},{6,30},{7,31}} | collective-permute-start | bytes 208904 | tf_op jit(solution)/shard_map/ppermute | solution.py:496
  30.5 0.0 collective-permute-done.17.refs_6_
  30.5 1.3 %collective-permute-start.12 = (s16[272,128]{1,0:T(8,128)(2,1)S(1)}, s16[272,128]{1,0:T(8,128)(2,1)S(1)}, u32[]{:S(2)}, u32[]{:S(2)}) collective-permute-start(s16[272,128]{1,0:T(8,128)(2,1)S(1)} %level_states_1.1.refs_7_), channel_id=1, source_target_pairs={{0,16},{8,24},{1,17},{9,25},{2,18},{10,26},{3,19},{11,27},{4,20},{... | collective-permute-start | bytes 208904 | tf_op jit(solution)/shard_map/ppermute | solution.py:496
  31.8 0.0 collective-permute-done.16.refs_5_
  31.8 0.2 carries_0.1
  32.0 1.9 %collective-permute-start.21 = (s16[272,128]{1,0:T(8,128)(2,1)S(1)}, s16[272,128]{1,0:T(8,128)(2,1)S(1)}, u32[]{:S(2)}, u32[]{:S(2)}) collective-permute-start(s16[272,128]{1,0:T(8,128)(2,1)S(1)} %get-tuple-element.65), channel_id=1, source_target_pairs={{0,6},{2,4},{4,2},{6,0},{1,7},{3,5},{5,3},{7,1},{8,14},{10,12},{12... | collective-permute-start | bytes 208904 | tf_op jit(solution)/shard_map/ppermute | solution.py:489
  33.9 0.5 collective-permute-start.20
  34.4 0.0 collective-permute-done.14.refs_6_.refs_13_
  34.4 0.0 collective-permute-done.13.refs_5_.refs_12_
  34.4 0.0 collective-permute-done.12.refs_4_.refs_11_
  34.4 0.2 carries_1.1
  34.6 2.3 %collective-permute-start.19 = (s16[272,128]{1,0:T(8,128)(2,1)S(1)}, s16[272,128]{1,0:T(8,128)(2,1)S(1)}, u32[]{:S(2)}, u32[]{:S(2)}) collective-permute-start(s16[272,128]{1,0:T(8,128)(2,1)S(1)} %get-tuple-element.63), channel_id=1, source_target_pairs={{0,6},{2,4},{4,2},{6,0},{1,7},{3,5},{5,3},{7,1},{8,14},{10,12},{12... | collective-permute-start | bytes 208904 | tf_op jit(solution)/shard_map/ppermute | solution.py:489
  36.9 0.4 collective-permute-start.18
  37.3 0.0 collective-permute-done.21.refs_9_
  37.3 1.1 %collective-permute-done.20.refs_8_ = s16[272,128]{1,0:T(8,128)(2,1)S(1)} collective-permute-done((s16[272,128]{1,0:T(8,128)(2,1)S(1)}, s16[272,128]{1,0:T(8,128)(2,1)S(1)}, u32[]{:S(2)}, u32[]{:S(2)}) %collective-permute-start.20) | collective-permute-done | bytes 69664 | tf_op jit(solution)/shard_map/ppermute | solution.py:489
  38.5 1.3 %attend_0_1_3.1.refs_10_ = bf16[512,512]{1,0:T(8,128)(2,1)S(1)} custom-call(bf16[256,1024]{1,0:T(8,128)(2,1)S(1)} %get-tuple-element.50.refs_5_.refs_0_, bf16[256,1024]{1,0:T(8,128)(2,1)S(1)} %collective-permute-done.5.refs_5_.refs_4_.refs_1_, bf16[256,1024]{1,0:T(8,128)(2,1)S(1)} %get-tuple-element.46.refs_0_.refs_2_, ...), custom_call_target="tpu_custom_call" | custom-call | flops 402653184 | bytes 2097152 | tf_op jit(solution)/shard_map/attend_0_1_3/pallas_call | solution.py:415
  39.8 1.2 %collective-permute-start.24 = (bf16[512,512]{1,0:T(8,128)(2,1)S(1)}, bf16[512,512]{1,0:T(8,128)(2,1)S(1)}, u32[]{:S(2)}, u32[]{:S(2)}) collective-permute-start(bf16[512,512]{1,0:T(8,128)(2,1)S(1)} %attend_0_1_3.1.refs_10_), channel_id=1, source_target_pairs={{0,2},{2,0},{1,3},{3,1},{4,6},{6,4},{5,7},{7,5},{8,10},{10,8},{9,1... | collective-permute-start | bytes 1572872 | tf_op jit(solution)/shard_map/ppermute | solution.py:489
  41.0 0.0 collective-permute-done.19.refs_9_
  41.0 1.0 %collective-permute-done.18.refs_8_ = s16[272,128]{1,0:T(8,128)(2,1)S(1)} collective-permute-done((s16[272,128]{1,0:T(8,128)(2,1)S(1)}, s16[272,128]{1,0:T(8,128)(2,1)S(1)}, u32[]{:S(2)}, u32[]{:S(2)}) %collective-permute-start.18) | collective-permute-done | bytes 69664 | tf_op jit(solution)/shard_map/ppermute | solution.py:489
  42.0 1.3 %attend_1_1_3.1.refs_14_.refs_10_ = bf16[512,512]{1,0:T(8,128)(2,1)S(1)} custom-call(bf16[256,1024]{1,0:T(8,128)(2,1)S(1)} %get-tuple-element.40.refs_0_, bf16[256,1024]{1,0:T(8,128)(2,1)S(1)} %collective-permute-done.refs_6_.refs_5_.refs_1_, bf16[256,1024]{1,0:T(8,128)(2,1)S(1)} %get-tuple-element.42.refs_0_.refs_2_, ...), custom_call_target="tpu_custom_call" | custom-call | flops 402653184 | bytes 2097152 | tf_op jit(solution)/shard_map/attend_1_1_3/pallas_call | solution.py:415
  43.4 1.0 %collective-permute-start.22 = (bf16[512,512]{1,0:T(8,128)(2,1)S(1)}, bf16[512,512]{1,0:T(8,128)(2,1)S(1)}, u32[]{:S(2)}, u32[]{:S(2)}) collective-permute-start(bf16[512,512]{1,0:T(8,128)(2,1)S(1)} %attend_1_1_3.1.refs_14_.refs_10_), channel_id=1, source_target_pairs={{0,2},{2,0},{1,3},{3,1},{4,6},{6,4},{5,7},{7,5},{8,10},{10,8},{9,1... | collective-permute-start | bytes 1572872 | tf_op jit(solution)/shard_map/ppermute | solution.py:489
  44.4 0.6 own_carries.1
  45.0 1.0 %collective-permute-start.25 = (f32[2,2,128,128]{3,2,1,0:T(8,128)S(1)}, f32[2,2,128,128]{3,2,1,0:T(8,128)S(1)}, u32[]{:S(2)}, u32[]{:S(2)}) collective-permute-start(f32[2,2,128,128]{3,2,1,0:T(8,128)S(1)} %get-tuple-element.69), channel_id=1, source_target_pairs={{0,4},{4,0},{1,5},{5,1},{2,6},{6,2},{3,7},{7,3},{8,12},{12,8},{9,1... | collective-permute-start | bytes 786440 | tf_op jit(solution)/shard_map/ppermute | solution.py:489
  46.0 1.1 %collective-permute-start.23 = (s16[528,128]{1,0:T(8,128)(2,1)S(1)}, s16[528,128]{1,0:T(8,128)(2,1)S(1)}, u32[]{:S(2)}, u32[]{:S(2)}) collective-permute-start(s16[528,128]{1,0:T(8,128)(2,1)S(1)} %get-tuple-element.67), channel_id=1, source_target_pairs={{0,4},{2,6},{4,0},{6,2},{1,5},{3,7},{5,1},{7,3},{8,12},{10,14},{12... | collective-permute-start | bytes 405512 | tf_op jit(solution)/shard_map/ppermute | solution.py:489
  47.0 5.8 %collective-permute-done.23.refs_9_ = s16[528,128]{1,0:T(8,128)(2,1)S(1)} collective-permute-done((s16[528,128]{1,0:T(8,128)(2,1)S(1)}, s16[528,128]{1,0:T(8,128)(2,1)S(1)}, u32[]{:S(2)}, u32[]{:S(2)}) %collective-permute-start.23) | collective-permute-done | bytes 135200 | tf_op jit(solution)/shard_map/ppermute | solution.py:489
  52.8 1.3 %attend_0_0_2.1.refs_10_.refs_0_ = bf16[512,512]{1,0:T(8,128)(2,1)S(1)} custom-call(bf16[256,1024]{1,0:T(8,128)(2,1)S(1)} %get-tuple-element.50.refs_5_.refs_0_, bf16[256,1024]{1,0:T(8,128)(2,1)S(1)} %collective-permute-done.5.refs_5_.refs_4_.refs_1_, bf16[256,1024]{1,0:T(8,128)(2,1)S(1)} %get-tuple-element.46.refs_0_.refs_2_, ...), custom_call_target="tpu_custom_call" | custom-call | flops 402653184 | bytes 2097152 | tf_op jit(solution)/shard_map/attend_0_0_2/pallas_call | solution.py:415
  54.2 1.3 %attend_1_0_2.1.refs_1_ = bf16[512,512]{1,0:T(8,128)(2,1)S(1)} custom-call(bf16[256,1024]{1,0:T(8,128)(2,1)S(1)} %get-tuple-element.40.refs_0_, bf16[256,1024]{1,0:T(8,128)(2,1)S(1)} %collective-permute-done.refs_6_.refs_5_.refs_1_, bf16[256,1024]{1,0:T(8,128)(2,1)S(1)} %get-tuple-element.42.refs_0_.refs_2_, ...), custom_call_target="tpu_custom_call" | custom-call | flops 402653184 | bytes 2097152 | tf_op jit(solution)/shard_map/attend_1_0_2/pallas_call | solution.py:415
  55.5 0.0 collective-permute-done.25.refs_1_
  55.5 0.8 %assemble_cache.1 = f32[1,8,128,128]{3,2,1,0:T(8,128)} custom-call(f32[2,2,128,128]{3,2,1,0:T(8,128)S(1)} %get-tuple-element.68.refs_0_, f32[2,2,128,128]{3,2,1,0:T(8,128)S(1)} %collective-permute-done.25.refs_1_), custom_call_target="tpu_custom_call" | custom-call | tf_op jit(solution)/shard_map/assemble_cache/pallas_call | solution.py:475
  56.4 1.2 %assemble.1.refs_1_ = bf16[1024,1024]{1,0:T(8,128)(2,1)} custom-call(bf16[512,512]{1,0:T(8,128)(2,1)S(1)} %attend_0_0_2.1.refs_10_.refs_0_, bf16[512,512]{1,0:T(8,128)(2,1)S(1)} %attend_1_0_2.1.refs_1_, bf16[512,512]{1,0:T(8,128)(2,1)S(1)} %collective-permute-done.24.refs_2_), custom_call_target="tpu_custom_call" | custom-call | tf_op jit(solution)/shard_map/assemble/pallas_call | solution.py:454
  57.5 5.1 %collective-permute-done.22.refs_0_ = bf16[512,512]{1,0:T(8,128)(2,1)S(1)} collective-permute-done((bf16[512,512]{1,0:T(8,128)(2,1)S(1)}, bf16[512,512]{1,0:T(8,128)(2,1)S(1)}, u32[]{:S(2)}, u32[]{:S(2)}) %collective-permute-start.22) | collective-permute-done | bytes 524320 | tf_op jit(solution)/shard_map/ppermute | solution.py:489
  62.6 0.8 %finish.1 = bf16[1024,1024]{1,0:T(8,128)(2,1)} custom-call(bf16[512,512]{1,0:T(8,128)(2,1)S(1)} %collective-permute-done.22.refs_0_, bf16[1024,1024]{1,0:T(8,128)(2,1)} %assemble.1.refs_1_), custom_call_target="tpu_custom_call", output_to_operand_aliasing={{}: (1, {})} | custom-call | tf_op jit(solution)/shard_map/finish/pallas_call | solution.py:454
  (8 shorter events, 0.0 us)
Async XLA Ops:
  0.6 4.7 %copy-start = (bf16[256,4096]{1,0:T(8,128)(2,1)S(1)}, bf16[256,4096]{1,0:T(8,128)(2,1)}, u32[]{:S(2)}) copy-start(bf16[256,4096]{1,0:T(8,128)(2,1)} %refs_0_.3) | copy-start | bytes 6291460
  4.7 2.1 %collective-permute-start.3 = (bf16[256,1024]{1,0:T(8,128)(2,1)S(1)}, bf16[256,1024]{1,0:T(8,128)(2,1)S(1)}, u32[]{:S(2)}, u32[]{:S(2)}) collective-permute-start(bf16[256,1024]{1,0:T(8,128)(2,1)S(1)} %get-tuple-element.47), channel_id=1, source_target_pairs={{0,1},{1,0},{2,3},{3,2},{4,5},{5,4},{6,7},{7,6},{8,9},{9,8},{10,11... | collective-permute-start | bytes 1572872 | tf_op jit(solution)/shard_map/ppermute | solution.py:489
  5.2 2.3 %collective-permute-start.4 = (bf16[256,1024]{1,0:T(8,128)(2,1)S(1)}, bf16[256,1024]{1,0:T(8,128)(2,1)S(1)}, u32[]{:S(2)}, u32[]{:S(2)}) collective-permute-start(bf16[256,1024]{1,0:T(8,128)(2,1)S(1)} %get-tuple-element.49), channel_id=1, source_target_pairs={{0,1},{1,0},{2,3},{3,2},{4,5},{5,4},{6,7},{7,6},{8,9},{9,8},{10,11... | collective-permute-start | bytes 1572872 | tf_op jit(solution)/shard_map/ppermute | solution.py:489
  5.3 2.2 %copy-start.1 = (f32[1024]{0:T(1024)S(1)}, f32[1024]{0:T(1024)}, u32[]{:S(2)}) copy-start(f32[1024]{0:T(1024)} %param.9) | copy-start | bytes 12292
  5.6 5.7 %collective-permute-start = (bf16[256,1024]{1,0:T(8,128)(2,1)S(1)}, bf16[256,1024]{1,0:T(8,128)(2,1)S(1)}, u32[]{:S(2)}, u32[]{:S(2)}) collective-permute-start(bf16[256,1024]{1,0:T(8,128)(2,1)S(1)} %get-tuple-element.41), channel_id=1, source_target_pairs={{0,1},{1,0},{2,3},{3,2},{4,5},{5,4},{6,7},{7,6},{8,9},{9,8},{10,11... | collective-permute-start | bytes 1572872 | tf_op jit(solution)/shard_map/ppermute | solution.py:489
  6.1 6.6 %collective-permute-start.5 = (bf16[256,1024]{1,0:T(8,128)(2,1)S(1)}, bf16[256,1024]{1,0:T(8,128)(2,1)S(1)}, u32[]{:S(2)}, u32[]{:S(2)}) collective-permute-start(bf16[256,1024]{1,0:T(8,128)(2,1)S(1)} %get-tuple-element.52), channel_id=1, source_target_pairs={{0,1},{1,0},{2,3},{3,2},{4,5},{5,4},{6,7},{7,6},{8,9},{9,8},{10,11... | collective-permute-start | bytes 1572872 | tf_op jit(solution)/shard_map/ppermute | solution.py:489
  6.2 6.7 %collective-permute-start.1 = (bf16[256,1024]{1,0:T(8,128)(2,1)S(1)}, bf16[256,1024]{1,0:T(8,128)(2,1)S(1)}, u32[]{:S(2)}, u32[]{:S(2)}) collective-permute-start(bf16[256,1024]{1,0:T(8,128)(2,1)S(1)} %get-tuple-element.43), channel_id=1, source_target_pairs={{0,1},{1,0},{2,3},{3,2},{4,5},{5,4},{6,7},{7,6},{8,9},{9,8},{10,11... | collective-permute-start | bytes 1572872 | tf_op jit(solution)/shard_map/ppermute | solution.py:489
  6.8 6.1 %collective-permute-start.2 = (bf16[256,1024]{1,0:T(8,128)(2,1)S(1)}, bf16[256,1024]{1,0:T(8,128)(2,1)S(1)}, u32[]{:S(2)}, u32[]{:S(2)}) collective-permute-start(bf16[256,1024]{1,0:T(8,128)(2,1)S(1)} %get-tuple-element.45), channel_id=1, source_target_pairs={{0,1},{1,0},{2,3},{3,2},{4,5},{5,4},{6,7},{7,6},{8,9},{9,8},{10,11... | collective-permute-start | bytes 1572872 | tf_op jit(solution)/shard_map/ppermute | solution.py:489
  8.3 10.0 %collective-permute-start.6 = (s16[288,128]{1,0:T(8,128)(2,1)S(1)}, s16[288,128]{1,0:T(8,128)(2,1)S(1)}, u32[]{:S(2)}, u32[]{:S(2)}) collective-permute-start(s16[288,128]{1,0:T(8,128)(2,1)S(1)} %get-tuple-element.54), channel_id=1, source_target_pairs={{0,2},{2,0},{4,6},{6,4},{1,3},{3,1},{5,7},{7,5},{8,10},{10,8},{12,... | collective-permute-start | bytes 221192 | tf_op jit(solution)/shard_map/ppermute | solution.py:489
  11.3 5.9 %collective-permute-start.10 = (s16[272,128]{1,0:T(8,128)(2,1)S(1)}, s16[272,128]{1,0:T(8,128)(2,1)S(1)}, u32[]{:S(2)}, u32[]{:S(2)}) collective-permute-start(s16[272,128]{1,0:T(8,128)(2,1)S(1)} %get-tuple-element.59), channel_id=1, source_target_pairs={{0,6},{2,4},{4,2},{6,0},{1,7},{3,5},{5,3},{7,1},{8,14},{10,12},{12... | collective-permute-start | bytes 208904 | tf_op jit(solution)/shard_map/ppermute | solution.py:489
  12.7 5.6 %collective-permute-start.11 = (s16[272,128]{1,0:T(8,128)(2,1)S(1)}, s16[272,128]{1,0:T(8,128)(2,1)S(1)}, u32[]{:S(2)}, u32[]{:S(2)}) collective-permute-start(s16[272,128]{1,0:T(8,128)(2,1)S(1)} %get-tuple-element.60), channel_id=1, source_target_pairs={{0,4},{2,6},{4,0},{6,2},{1,5},{3,7},{5,1},{7,3},{8,12},{10,14},{12... | collective-permute-start | bytes 208904 | tf_op jit(solution)/shard_map/ppermute | solution.py:489
  13.7 11.6 %collective-permute-start.7 = (s16[272,128]{1,0:T(8,128)(2,1)S(1)}, s16[272,128]{1,0:T(8,128)(2,1)S(1)}, u32[]{:S(2)}, u32[]{:S(2)}) collective-permute-start(s16[272,128]{1,0:T(8,128)(2,1)S(1)} %get-tuple-element.56), channel_id=1, source_target_pairs={{0,2},{2,0},{4,6},{6,4},{1,3},{3,1},{5,7},{7,5},{8,10},{10,8},{12,... | collective-permute-start | bytes 208904 | tf_op jit(solution)/shard_map/ppermute | solution.py:489
  15.7 11.4 %collective-permute-start.8 = (s16[272,128]{1,0:T(8,128)(2,1)S(1)}, s16[272,128]{1,0:T(8,128)(2,1)S(1)}, u32[]{:S(2)}, u32[]{:S(2)}) collective-permute-start(s16[272,128]{1,0:T(8,128)(2,1)S(1)} %get-tuple-element.57), channel_id=1, source_target_pairs={{0,4},{2,6},{4,0},{6,2},{1,5},{3,7},{5,1},{7,3},{8,12},{10,14},{12... | collective-permute-start | bytes 208904 | tf_op jit(solution)/shard_map/ppermute | solution.py:489
  17.2 9.9 %collective-permute-start.9 = (s16[272,128]{1,0:T(8,128)(2,1)S(1)}, s16[272,128]{1,0:T(8,128)(2,1)S(1)}, u32[]{:S(2)}, u32[]{:S(2)}) collective-permute-start(s16[272,128]{1,0:T(8,128)(2,1)S(1)} %get-tuple-element.58), channel_id=1, source_target_pairs={{0,6},{2,4},{4,2},{6,0},{1,7},{3,5},{5,3},{7,1},{8,14},{10,12},{12... | collective-permute-start | bytes 208904 | tf_op jit(solution)/shard_map/ppermute | solution.py:489
  18.4 12.0 %collective-permute-start.17 = (s16[272,128]{1,0:T(8,128)(2,1)S(1)}, s16[272,128]{1,0:T(8,128)(2,1)S(1)}, u32[]{:S(2)}, u32[]{:S(2)}) collective-permute-start(s16[272,128]{1,0:T(8,128)(2,1)S(1)} %level_states_0.1.refs_3_), channel_id=1, source_target_pairs={{0,8},{8,16},{16,24},{1,9},{9,17},{17,25},{2,10},{10,18},{18,26},{... | collective-permute-start | bytes 208904 | tf_op jit(solution)/shard_map/ppermute | solution.py:496
  21.9 9.9 %collective-permute-start.16 = (s16[272,128]{1,0:T(8,128)(2,1)S(1)}, s16[272,128]{1,0:T(8,128)(2,1)S(1)}, u32[]{:S(2)}, u32[]{:S(2)}) collective-permute-start(s16[272,128]{1,0:T(8,128)(2,1)S(1)} %level_states_0.1.refs_3_), channel_id=1, source_target_pairs={{0,24},{1,25},{2,26},{3,27},{4,28},{5,29},{6,30},{7,31}} | collective-permute-start | bytes 208904 | tf_op jit(solution)/shard_map/ppermute | solution.py:496
  25.2 6.5 %collective-permute-start.15 = (s16[272,128]{1,0:T(8,128)(2,1)S(1)}, s16[272,128]{1,0:T(8,128)(2,1)S(1)}, u32[]{:S(2)}, u32[]{:S(2)}) collective-permute-start(s16[272,128]{1,0:T(8,128)(2,1)S(1)} %level_states_0.1.refs_3_), channel_id=1, source_target_pairs={{0,16},{8,24},{1,17},{9,25},{2,18},{10,26},{3,19},{11,27},{4,20},{... | collective-permute-start | bytes 208904 | tf_op jit(solution)/shard_map/ppermute | solution.py:496
  27.2 7.2 %collective-permute-start.14 = (s16[272,128]{1,0:T(8,128)(2,1)S(1)}, s16[272,128]{1,0:T(8,128)(2,1)S(1)}, u32[]{:S(2)}, u32[]{:S(2)}) collective-permute-start(s16[272,128]{1,0:T(8,128)(2,1)S(1)} %level_states_1.1.refs_7_), channel_id=1, source_target_pairs={{0,8},{8,16},{16,24},{1,9},{9,17},{17,25},{2,10},{10,18},{18,26},{... | collective-permute-start | bytes 208904 | tf_op jit(solution)/shard_map/ppermute | solution.py:496
  29.2 5.2 %collective-permute-start.13 = (s16[272,128]{1,0:T(8,128)(2,1)S(1)}, s16[272,128]{1,0:T(8,128)(2,1)S(1)}, u32[]{:S(2)}, u32[]{:S(2)}) collective-permute-start(s16[272,128]{1,0:T(8,128)(2,1)S(1)} %level_states_1.1.refs_7_), channel_id=1, source_target_pairs={{0,24},{1,25},{2,26},{3,27},{4,28},{5,29},{6,30},{7,31}} | collective-permute-start | bytes 208904 | tf_op jit(solution)/shard_map/ppermute | solution.py:496
  30.5 3.9 %collective-permute-start.12 = (s16[272,128]{1,0:T(8,128)(2,1)S(1)}, s16[272,128]{1,0:T(8,128)(2,1)S(1)}, u32[]{:S(2)}, u32[]{:S(2)}) collective-permute-start(s16[272,128]{1,0:T(8,128)(2,1)S(1)} %level_states_1.1.refs_7_), channel_id=1, source_target_pairs={{0,16},{8,24},{1,17},{9,25},{2,18},{10,26},{3,19},{11,27},{4,20},{... | collective-permute-start | bytes 208904 | tf_op jit(solution)/shard_map/ppermute | solution.py:496
  32.0 5.3 %collective-permute-start.21 = (s16[272,128]{1,0:T(8,128)(2,1)S(1)}, s16[272,128]{1,0:T(8,128)(2,1)S(1)}, u32[]{:S(2)}, u32[]{:S(2)}) collective-permute-start(s16[272,128]{1,0:T(8,128)(2,1)S(1)} %get-tuple-element.65), channel_id=1, source_target_pairs={{0,6},{2,4},{4,2},{6,0},{1,7},{3,5},{5,3},{7,1},{8,14},{10,12},{12... | collective-permute-start | bytes 208904 | tf_op jit(solution)/shard_map/ppermute | solution.py:489
  33.9 4.6 %collective-permute-start.20 = (s16[272,128]{1,0:T(8,128)(2,1)S(1)}, s16[272,128]{1,0:T(8,128)(2,1)S(1)}, u32[]{:S(2)}, u32[]{:S(2)}) collective-permute-start(s16[272,128]{1,0:T(8,128)(2,1)S(1)} %get-tuple-element.61.refs_7_), channel_id=1, source_target_pairs={{0,2},{2,0},{4,6},{6,4},{1,3},{3,1},{5,7},{7,5},{8,10},{10,8},{12,... | collective-permute-start | bytes 208904 | tf_op jit(solution)/shard_map/ppermute | solution.py:489
  34.6 6.4 %collective-permute-start.19 = (s16[272,128]{1,0:T(8,128)(2,1)S(1)}, s16[272,128]{1,0:T(8,128)(2,1)S(1)}, u32[]{:S(2)}, u32[]{:S(2)}) collective-permute-start(s16[272,128]{1,0:T(8,128)(2,1)S(1)} %get-tuple-element.63), channel_id=1, source_target_pairs={{0,6},{2,4},{4,2},{6,0},{1,7},{3,5},{5,3},{7,1},{8,14},{10,12},{12... | collective-permute-start | bytes 208904 | tf_op jit(solution)/shard_map/ppermute | solution.py:489
  36.9 5.1 %collective-permute-start.18 = (s16[272,128]{1,0:T(8,128)(2,1)S(1)}, s16[272,128]{1,0:T(8,128)(2,1)S(1)}, u32[]{:S(2)}, u32[]{:S(2)}) collective-permute-start(s16[272,128]{1,0:T(8,128)(2,1)S(1)} %get-tuple-element.62.refs_10_), channel_id=1, source_target_pairs={{0,2},{2,0},{4,6},{6,4},{1,3},{3,1},{5,7},{7,5},{8,10},{10,8},{12,... | collective-permute-start | bytes 208904 | tf_op jit(solution)/shard_map/ppermute | solution.py:489
  39.8 16.5 %collective-permute-start.24 = (bf16[512,512]{1,0:T(8,128)(2,1)S(1)}, bf16[512,512]{1,0:T(8,128)(2,1)S(1)}, u32[]{:S(2)}, u32[]{:S(2)}) collective-permute-start(bf16[512,512]{1,0:T(8,128)(2,1)S(1)} %attend_0_1_3.1.refs_10_), channel_id=1, source_target_pairs={{0,2},{2,0},{1,3},{3,1},{4,6},{6,4},{5,7},{7,5},{8,10},{10,8},{9,1... | collective-permute-start | bytes 1572872 | tf_op jit(solution)/shard_map/ppermute | solution.py:489
  43.4 19.2 %collective-permute-start.22 = (bf16[512,512]{1,0:T(8,128)(2,1)S(1)}, bf16[512,512]{1,0:T(8,128)(2,1)S(1)}, u32[]{:S(2)}, u32[]{:S(2)}) collective-permute-start(bf16[512,512]{1,0:T(8,128)(2,1)S(1)} %attend_1_1_3.1.refs_14_.refs_10_), channel_id=1, source_target_pairs={{0,2},{2,0},{1,3},{3,1},{4,6},{6,4},{5,7},{7,5},{8,10},{10,8},{9,1... | collective-permute-start | bytes 1572872 | tf_op jit(solution)/shard_map/ppermute | solution.py:489
  45.0 10.5 %collective-permute-start.25 = (f32[2,2,128,128]{3,2,1,0:T(8,128)S(1)}, f32[2,2,128,128]{3,2,1,0:T(8,128)S(1)}, u32[]{:S(2)}, u32[]{:S(2)}) collective-permute-start(f32[2,2,128,128]{3,2,1,0:T(8,128)S(1)} %get-tuple-element.69), channel_id=1, source_target_pairs={{0,4},{4,0},{1,5},{5,1},{2,6},{6,2},{3,7},{7,3},{8,12},{12,8},{9,1... | collective-permute-start | bytes 786440 | tf_op jit(solution)/shard_map/ppermute | solution.py:489
  46.0 6.9 %collective-permute-start.23 = (s16[528,128]{1,0:T(8,128)(2,1)S(1)}, s16[528,128]{1,0:T(8,128)(2,1)S(1)}, u32[]{:S(2)}, u32[]{:S(2)}) collective-permute-start(s16[528,128]{1,0:T(8,128)(2,1)S(1)} %get-tuple-element.67), channel_id=1, source_target_pairs={{0,4},{2,6},{4,0},{6,2},{1,5},{3,7},{5,1},{7,3},{8,12},{10,14},{12... | collective-permute-start | bytes 405512 | tf_op jit(solution)/shard_map/ppermute | solution.py:489
